TPU v7x, 8 devices: a whole 2x2x1 slice. The times are simulated.
8 devices in a mesh: dp: 1 (over z), cp: 2 (over y), tp: 4 (over x, core).
Axes of the slice: x: 2, y: 2, z: 1, core: 2. Of those that a mesh axis runs over, the one named last changes fastest.
Arguments:
- x: bfloat16 [1, 8192, 4096], P('dp', ('cp', 'tp'))
- g_attn: bfloat16 [4096], replicated
- w_q: bfloat16 [4096, 32, 128], P(None, 'tp')
- w_k: bfloat16 [4096, 8, 128], P(None, 'tp')
- w_v: bfloat16 [4096, 8, 128], P(None, 'tp')
- w_o: bfloat16 [32, 128, 4096], P('tp')
- g_mlp: bfloat16 [4096], replicated
- w_gate: bfloat16 [4096, 12288], P(None, 'tp')
- w_up: bfloat16 [4096, 12288], P(None, 'tp')
- w_down: bfloat16 [12288, 4096], P('tp')
Outputs:
- output: bfloat16 [1, 8192, 4096], P('dp', ('cp', 'tp'))
All inputs are finite; a program needn't handle non-finite values.
Results may differ from a plain program's by a relative error of at most 0.02.
Values are sent between devices in bfloat16 or wider.
A program may use at most 1 GiB of HBM per device.

v0:
```python
import jax
import jax.numpy as jnp
from jax import lax
from jax.sharding import PartitionSpec as P

NORM_EPS = 1e-5
ROPE_THETA = 500000.0
TILE_ROWS = 256


def rms_norm(rows_in, gain_vec):
    rows_f32 = rows_in.astype(jnp.float32)
    mean_sq = jnp.mean(rows_f32 * rows_f32, axis=-1, keepdims=True)
    return (rows_f32 * lax.rsqrt(mean_sq + NORM_EPS) * gain_vec.astype(jnp.float32)).astype(jnp.bfloat16)


def apply_rope(heads_in, positions):
    head_dim = heads_in.shape[-1]
    half_dim = head_dim // 2
    inv_freq = ROPE_THETA ** (-2.0 * jnp.arange(half_dim, dtype=jnp.float32) / head_dim)
    angles = positions.astype(jnp.float32)[:, None] * inv_freq[None, :]
    angles = jnp.concatenate([angles, angles], axis=-1)[:, None, :]
    heads_f32 = heads_in.astype(jnp.float32)
    rotated = jnp.concatenate([-heads_f32[..., half_dim:], heads_f32[..., :half_dim]], axis=-1)
    return (heads_f32 * jnp.cos(angles) + rotated * jnp.sin(angles)).astype(jnp.bfloat16)


def stored_positions(row_ids, piece_len, cp_size):
    owner_cp = row_ids // (2 * piece_len)
    within = row_ids % (2 * piece_len)
    return jnp.where(within < piece_len, owner_cp * piece_len + within,
                     (2 * cp_size - 1 - owner_cp) * piece_len + within - piece_len)


def attend(q_rows, q_pos, keys, values, key_pos):
    q_len, n_kv_heads, group_size, head_dim = q_rows.shape
    n_tiles = max(1, q_len // TILE_ROWS)
    tile_len = q_len // n_tiles
    score_scale = head_dim ** -0.5

    def one_tile(tile_idx):
        row_start = tile_idx * tile_len
        q_tile = lax.dynamic_slice_in_dim(q_rows, row_start, tile_len, axis=0)
        pos_tile = lax.dynamic_slice_in_dim(q_pos, row_start, tile_len, axis=0)
        scores = jnp.einsum('qgrd,kgd->gqrk', q_tile, keys, preferred_element_type=jnp.float32) * score_scale
        visible = pos_tile[:, None, None] >= key_pos[None, None, :]
        scores = jnp.where(visible, scores, -1e30)
        weights = jnp.exp(scores - jnp.max(scores, axis=-1, keepdims=True))
        row_sum = jnp.sum(weights, axis=-1, keepdims=True)
        mixed_vals = jnp.einsum('gqrk,kgd->gqrd', weights.astype(jnp.bfloat16), values, preferred_element_type=jnp.float32) / row_sum
        return jnp.transpose(mixed_vals, (1, 0, 2, 3)).astype(jnp.bfloat16)

    tiles = lax.map(one_tile, jnp.arange(n_tiles))
    return tiles.reshape(q_len, n_kv_heads * group_size, head_dim)


def solution(mesh):
    cp_size = mesh.shape['cp']
    row_spec = P('dp', ('cp', 'tp'), None)
    head_cols = P(None, 'tp', None)

    def local_layer(x, g_attn, w_q, w_k, w_v, w_o, g_mlp, w_gate, w_up, w_down):
        x_rows = x[0]
        n_kv_local = w_k.shape[1]
        head_dim = w_q.shape[2]
        group_size = w_q.shape[1] // n_kv_local
        cp_index = lax.axis_index('cp')
        normed = lax.all_gather(rms_norm(x_rows, g_attn), 'tp', axis=0, tiled=True)
        seq_local = normed.shape[0]
        piece_len = seq_local // 2
        positions = stored_positions(cp_index * seq_local + jnp.arange(seq_local, dtype=jnp.int32), piece_len, cp_size)
        q_all = apply_rope(jnp.einsum('sd,dhk->shk', normed, w_q, preferred_element_type=jnp.float32).astype(jnp.bfloat16), positions)
        k_all = apply_rope(jnp.einsum('sd,dhk->shk', normed, w_k, preferred_element_type=jnp.float32).astype(jnp.bfloat16), positions)
        v_all = jnp.einsum('sd,dhk->shk', normed, w_v, preferred_element_type=jnp.float32).astype(jnp.bfloat16)
        k_seq = lax.all_gather(k_all, 'cp', axis=0, tiled=False)
        v_seq = lax.all_gather(v_all, 'cp', axis=0, tiled=False)
        key_pos = stored_positions(jnp.arange(cp_size * seq_local, dtype=jnp.int32), piece_len, cp_size).reshape(cp_size, seq_local)
        first_keys = k_seq[:, :piece_len].reshape(cp_size * piece_len, n_kv_local, head_dim)
        first_vals = v_seq[:, :piece_len].reshape(cp_size * piece_len, n_kv_local, head_dim)
        first_pos = key_pos[:, :piece_len].reshape(cp_size * piece_len)
        q_grp = q_all.reshape(seq_local, n_kv_local, group_size, head_dim)
        attn_first = attend(q_grp[:piece_len], positions[:piece_len], first_keys, first_vals, first_pos)
        attn_second = attend(q_grp[piece_len:], positions[piece_len:],
                             k_seq.reshape(cp_size * seq_local, n_kv_local, head_dim),
                             v_seq.reshape(cp_size * seq_local, n_kv_local, head_dim),
                             key_pos.reshape(cp_size * seq_local))
        attn_out = jnp.concatenate([attn_first, attn_second], axis=0)
        attn_part = jnp.einsum('shk,hkd->sd', attn_out, w_o, preferred_element_type=jnp.float32).astype(jnp.bfloat16)
        attn_rows = lax.psum_scatter(attn_part, 'tp', scatter_dimension=0, tiled=True)
        resid_rows = (x_rows.astype(jnp.float32) + attn_rows.astype(jnp.float32)).astype(jnp.bfloat16)
        normed_mlp = lax.all_gather(rms_norm(resid_rows, g_mlp), 'tp', axis=0, tiled=True)
        gate_proj = jnp.dot(normed_mlp, w_gate, preferred_element_type=jnp.float32)
        up_proj = jnp.dot(normed_mlp, w_up, preferred_element_type=jnp.float32)
        hidden = (jax.nn.silu(gate_proj) * up_proj).astype(jnp.bfloat16)
        down_part = jnp.dot(hidden, w_down, preferred_element_type=jnp.float32).astype(jnp.bfloat16)
        down_rows = lax.psum_scatter(down_part, 'tp', scatter_dimension=0, tiled=True)
        z_rows = (resid_rows.astype(jnp.float32) + down_rows.astype(jnp.float32)).astype(jnp.bfloat16)
        return z_rows[None]

    return jax.shard_map(local_layer, mesh=mesh,
                         in_specs=(row_spec, P(), head_cols, head_cols, head_cols, P('tp', None, None),
                                   P(), P(None, 'tp'), P(None, 'tp'), P('tp', None)),
                         out_specs=row_spec, check_vma=False)
```

profile of v0, /device:TPU:0, one launch (start us, length us, event | category | flops | bytes accessed | tf_op | source)
XLA Modules:
  0.0 2499.4 jit_solution(13320917544348113032)
XLA Ops:
  50.6 174.0 %all-gather.7.cloned.1.call-done = bf16[4096,4096]{1,0:T(8,128)(2,1)} async-done(((bf16[1024,4096]{1,0:T(8,128)(2,1)}), bf16[4096,4096]{1,0:T(8,128)(2,1)}) %all-gather.7.cloned.1.call-update) | async-done | bytes 33554448 | tf_op jit(solution)/shard_map/all_gather | solution.py:68
  224.7 16.8 fusion.103
  242.1 15.7 fusion.124
  262.7 43.3 %fusion.123 = f32[4096,1024]{0,1} fusion(bf16[4096,4096]{1,0:T(8,128)(2,1)} %all-gather.7.cloned.1.call-done, bf16[4096,1024]{0,1:T(8,128)(2,1)} %bitcast.159), kind=kOutput, calls=%fused_computation.131 | convolution fusion | flops 34359738368 | bytes 58720256
  375.8 647.7 %while.22 = (s32[]{:T(128)}, bf16[8,256,2,4,128]{4,1,0,3,2:T(8,128)(2,1)}, s32[8]{0:T(128)S(1)}, s32[2048]{0:T(1024)}, bf16[2048,2,4,128]{0,3,2,1:T(8,128)(2,1)}...) while((s32[]{:T(128)}, ...), condition=%wide.region_8.9_spmd.clone, body=%wide.region_5.8_spmd.clone.sunk | while | flops 8777265152 | bytes 219262128 | solution.py:53
  379.2 28.3 %fusion.160 = (f32[2,256,4]{1,2,0:T(4,128)S(1)}, f32[2,256,4,8192]{3,1,2,0:T(8,128)}) fusion(pred[256,8192]{1,0:T(8,128)(4,1)S(1)} %broadcast_compare_fusion.6, bf16[8192,2,128]{2,0,1:T(8,128)(2,1)} %get-tuple-element.314, bf16[2048,2,4,128]{0,3,2,1:T(8,128)(2,1)} %get-tuple-element.313, s32[]{:T(128)S(6)} %select_n.207), kind=kOutput, calls=%fused_computation.22.clone.1 | convolution fusion | flops 4345296896 | bytes 73932800 | tf_op jit(solution)/shard_map/while/body/eval_jaxpr/qgrd,kgd->gqrk/dot_general | solution.py:45
  407.5 21.6 fusion.161
  429.1 27.8 %fusion.162 = bf16[8,256,2,4,128]{4,1,0,3,2:T(8,128)(2,1)} fusion(bf16[8,256,2,4,128]{4,1,0,3,2:T(8,128)(2,1)} %get-tuple-element.299, s32[]{:T(128)S(6)} %copy.48, bf16[8192,2,128]{2,0,1:T(8,128)(2,1)} %get-tuple-element.315, f32[2,256,4,8192]{3,1,2,0:T(8,128)} %get-tuple-element.285, f32[2,256,4]{1,2,0:T(4,128)S(1)} %get-tuple-element.286, ...), kind=kOutput, calls=%fused_computation.35.clone.1 | convolution fusion | flops 4362600448 | bytes 73940992 | tf_op jit(solution)/shard_map/while/body/eval_jaxpr/gqrk,kgd->gqrd/dot_general | solution.py:50
  460.1 28.3 %fusion.160 = (f32[2,256,4]{1,2,0:T(4,128)S(1)}, f32[2,256,4,8192]{3,1,2,0:T(8,128)}) fusion(pred[256,8192]{1,0:T(8,128)(4,1)S(1)} %broadcast_compare_fusion.6, bf16[8192,2,128]{2,0,1:T(8,128)(2,1)} %get-tuple-element.314, bf16[2048,2,4,128]{0,3,2,1:T(8,128)(2,1)} %get-tuple-element.313, s32[]{:T(128)S(6)} %select_n.207), kind=kOutput, calls=%fused_computation.22.clone.1 | convolution fusion | flops 4345296896 | bytes 73932800 | tf_op jit(solution)/shard_map/while/body/eval_jaxpr/qgrd,kgd->gqrk/dot_general | solution.py:45
  488.4 21.6 fusion.161
  510.0 27.8 %fusion.162 = bf16[8,256,2,4,128]{4,1,0,3,2:T(8,128)(2,1)} fusion(bf16[8,256,2,4,128]{4,1,0,3,2:T(8,128)(2,1)} %get-tuple-element.299, s32[]{:T(128)S(6)} %copy.48, bf16[8192,2,128]{2,0,1:T(8,128)(2,1)} %get-tuple-element.315, f32[2,256,4,8192]{3,1,2,0:T(8,128)} %get-tuple-element.285, f32[2,256,4]{1,2,0:T(4,128)S(1)} %get-tuple-element.286, ...), kind=kOutput, calls=%fused_computation.35.clone.1 | convolution fusion | flops 4362600448 | bytes 73940992 | tf_op jit(solution)/shard_map/while/body/eval_jaxpr/gqrk,kgd->gqrd/dot_general | solution.py:50
  541.0 28.3 %fusion.160 = (f32[2,256,4]{1,2,0:T(4,128)S(1)}, f32[2,256,4,8192]{3,1,2,0:T(8,128)}) fusion(pred[256,8192]{1,0:T(8,128)(4,1)S(1)} %broadcast_compare_fusion.6, bf16[8192,2,128]{2,0,1:T(8,128)(2,1)} %get-tuple-element.314, bf16[2048,2,4,128]{0,3,2,1:T(8,128)(2,1)} %get-tuple-element.313, s32[]{:T(128)S(6)} %select_n.207), kind=kOutput, calls=%fused_computation.22.clone.1 | convolution fusion | flops 4345296896 | bytes 73932800 | tf_op jit(solution)/shard_map/while/body/eval_jaxpr/qgrd,kgd->gqrk/dot_general | solution.py:45
  569.3 21.6 fusion.161
  590.9 27.8 %fusion.162 = bf16[8,256,2,4,128]{4,1,0,3,2:T(8,128)(2,1)} fusion(bf16[8,256,2,4,128]{4,1,0,3,2:T(8,128)(2,1)} %get-tuple-element.299, s32[]{:T(128)S(6)} %copy.48, bf16[8192,2,128]{2,0,1:T(8,128)(2,1)} %get-tuple-element.315, f32[2,256,4,8192]{3,1,2,0:T(8,128)} %get-tuple-element.285, f32[2,256,4]{1,2,0:T(4,128)S(1)} %get-tuple-element.286, ...), kind=kOutput, calls=%fused_computation.35.clone.1 | convolution fusion | flops 4362600448 | bytes 73940992 | tf_op jit(solution)/shard_map/while/body/eval_jaxpr/gqrk,kgd->gqrd/dot_general | solution.py:50
  621.9 28.3 %fusion.160 = (f32[2,256,4]{1,2,0:T(4,128)S(1)}, f32[2,256,4,8192]{3,1,2,0:T(8,128)}) fusion(pred[256,8192]{1,0:T(8,128)(4,1)S(1)} %broadcast_compare_fusion.6, bf16[8192,2,128]{2,0,1:T(8,128)(2,1)} %get-tuple-element.314, bf16[2048,2,4,128]{0,3,2,1:T(8,128)(2,1)} %get-tuple-element.313, s32[]{:T(128)S(6)} %select_n.207), kind=kOutput, calls=%fused_computation.22.clone.1 | convolution fusion | flops 4345296896 | bytes 73932800 | tf_op jit(solution)/shard_map/while/body/eval_jaxpr/qgrd,kgd->gqrk/dot_general | solution.py:45
  650.2 21.6 fusion.161
  671.7 27.8 %fusion.162 = bf16[8,256,2,4,128]{4,1,0,3,2:T(8,128)(2,1)} fusion(bf16[8,256,2,4,128]{4,1,0,3,2:T(8,128)(2,1)} %get-tuple-element.299, s32[]{:T(128)S(6)} %copy.48, bf16[8192,2,128]{2,0,1:T(8,128)(2,1)} %get-tuple-element.315, f32[2,256,4,8192]{3,1,2,0:T(8,128)} %get-tuple-element.285, f32[2,256,4]{1,2,0:T(4,128)S(1)} %get-tuple-element.286, ...), kind=kOutput, calls=%fused_computation.35.clone.1 | convolution fusion | flops 4362600448 | bytes 73940992 | tf_op jit(solution)/shard_map/while/body/eval_jaxpr/gqrk,kgd->gqrd/dot_general | solution.py:50
  702.8 28.3 %fusion.160 = (f32[2,256,4]{1,2,0:T(4,128)S(1)}, f32[2,256,4,8192]{3,1,2,0:T(8,128)}) fusion(pred[256,8192]{1,0:T(8,128)(4,1)S(1)} %broadcast_compare_fusion.6, bf16[8192,2,128]{2,0,1:T(8,128)(2,1)} %get-tuple-element.314, bf16[2048,2,4,128]{0,3,2,1:T(8,128)(2,1)} %get-tuple-element.313, s32[]{:T(128)S(6)} %select_n.207), kind=kOutput, calls=%fused_computation.22.clone.1 | convolution fusion | flops 4345296896 | bytes 73932800 | tf_op jit(solution)/shard_map/while/body/eval_jaxpr/qgrd,kgd->gqrk/dot_general | solution.py:45
  731.0 21.6 fusion.161
  752.6 27.8 %fusion.162 = bf16[8,256,2,4,128]{4,1,0,3,2:T(8,128)(2,1)} fusion(bf16[8,256,2,4,128]{4,1,0,3,2:T(8,128)(2,1)} %get-tuple-element.299, s32[]{:T(128)S(6)} %copy.48, bf16[8192,2,128]{2,0,1:T(8,128)(2,1)} %get-tuple-element.315, f32[2,256,4,8192]{3,1,2,0:T(8,128)} %get-tuple-element.285, f32[2,256,4]{1,2,0:T(4,128)S(1)} %get-tuple-element.286, ...), kind=kOutput, calls=%fused_computation.35.clone.1 | convolution fusion | flops 4362600448 | bytes 73940992 | tf_op jit(solution)/shard_map/while/body/eval_jaxpr/gqrk,kgd->gqrd/dot_general | solution.py:50
  783.7 28.3 %fusion.160 = (f32[2,256,4]{1,2,0:T(4,128)S(1)}, f32[2,256,4,8192]{3,1,2,0:T(8,128)}) fusion(pred[256,8192]{1,0:T(8,128)(4,1)S(1)} %broadcast_compare_fusion.6, bf16[8192,2,128]{2,0,1:T(8,128)(2,1)} %get-tuple-element.314, bf16[2048,2,4,128]{0,3,2,1:T(8,128)(2,1)} %get-tuple-element.313, s32[]{:T(128)S(6)} %select_n.207), kind=kOutput, calls=%fused_computation.22.clone.1 | convolution fusion | flops 4345296896 | bytes 73932800 | tf_op jit(solution)/shard_map/while/body/eval_jaxpr/qgrd,kgd->gqrk/dot_general | solution.py:45
  811.9 21.6 fusion.161
  833.5 27.8 %fusion.162 = bf16[8,256,2,4,128]{4,1,0,3,2:T(8,128)(2,1)} fusion(bf16[8,256,2,4,128]{4,1,0,3,2:T(8,128)(2,1)} %get-tuple-element.299, s32[]{:T(128)S(6)} %copy.48, bf16[8192,2,128]{2,0,1:T(8,128)(2,1)} %get-tuple-element.315, f32[2,256,4,8192]{3,1,2,0:T(8,128)} %get-tuple-element.285, f32[2,256,4]{1,2,0:T(4,128)S(1)} %get-tuple-element.286, ...), kind=kOutput, calls=%fused_computation.35.clone.1 | convolution fusion | flops 4362600448 | bytes 73940992 | tf_op jit(solution)/shard_map/while/body/eval_jaxpr/gqrk,kgd->gqrd/dot_general | solution.py:50
  864.5 28.3 %fusion.160 = (f32[2,256,4]{1,2,0:T(4,128)S(1)}, f32[2,256,4,8192]{3,1,2,0:T(8,128)}) fusion(pred[256,8192]{1,0:T(8,128)(4,1)S(1)} %broadcast_compare_fusion.6, bf16[8192,2,128]{2,0,1:T(8,128)(2,1)} %get-tuple-element.314, bf16[2048,2,4,128]{0,3,2,1:T(8,128)(2,1)} %get-tuple-element.313, s32[]{:T(128)S(6)} %select_n.207), kind=kOutput, calls=%fused_computation.22.clone.1 | convolution fusion | flops 4345296896 | bytes 73932800 | tf_op jit(solution)/shard_map/while/body/eval_jaxpr/qgrd,kgd->gqrk/dot_general | solution.py:45
  892.8 21.6 fusion.161
  914.4 27.8 %fusion.162 = bf16[8,256,2,4,128]{4,1,0,3,2:T(8,128)(2,1)} fusion(bf16[8,256,2,4,128]{4,1,0,3,2:T(8,128)(2,1)} %get-tuple-element.299, s32[]{:T(128)S(6)} %copy.48, bf16[8192,2,128]{2,0,1:T(8,128)(2,1)} %get-tuple-element.315, f32[2,256,4,8192]{3,1,2,0:T(8,128)} %get-tuple-element.285, f32[2,256,4]{1,2,0:T(4,128)S(1)} %get-tuple-element.286, ...), kind=kOutput, calls=%fused_computation.35.clone.1 | convolution fusion | flops 4362600448 | bytes 73940992 | tf_op jit(solution)/shard_map/while/body/eval_jaxpr/gqrk,kgd->gqrd/dot_general | solution.py:50
  945.4 28.3 %fusion.160 = (f32[2,256,4]{1,2,0:T(4,128)S(1)}, f32[2,256,4,8192]{3,1,2,0:T(8,128)}) fusion(pred[256,8192]{1,0:T(8,128)(4,1)S(1)} %broadcast_compare_fusion.6, bf16[8192,2,128]{2,0,1:T(8,128)(2,1)} %get-tuple-element.314, bf16[2048,2,4,128]{0,3,2,1:T(8,128)(2,1)} %get-tuple-element.313, s32[]{:T(128)S(6)} %select_n.207), kind=kOutput, calls=%fused_computation.22.clone.1 | convolution fusion | flops 4345296896 | bytes 73932800 | tf_op jit(solution)/shard_map/while/body/eval_jaxpr/qgrd,kgd->gqrk/dot_general | solution.py:45
  973.7 21.6 fusion.161
  995.3 27.8 %fusion.162 = bf16[8,256,2,4,128]{4,1,0,3,2:T(8,128)(2,1)} fusion(bf16[8,256,2,4,128]{4,1,0,3,2:T(8,128)(2,1)} %get-tuple-element.299, s32[]{:T(128)S(6)} %copy.48, bf16[8192,2,128]{2,0,1:T(8,128)(2,1)} %get-tuple-element.315, f32[2,256,4,8192]{3,1,2,0:T(8,128)} %get-tuple-element.285, f32[2,256,4]{1,2,0:T(4,128)S(1)} %get-tuple-element.286, ...), kind=kOutput, calls=%fused_computation.35.clone.1 | convolution fusion | flops 4362600448 | bytes 73940992 | tf_op jit(solution)/shard_map/while/body/eval_jaxpr/gqrk,kgd->gqrd/dot_general | solution.py:50
  1026.5 389.2 %while.21 = (s32[]{:T(128)}, bf16[8,256,2,4,128]{4,1,0,3,2:T(8,128)(2,1)}, s32[8]{0:T(128)S(1)}, s32[2048]{0:T(1024)}, s32[2,2048]{1,0:T(2,128)S(1)}, /*index=5*...) while((s32[]{:T(128)}, ...), condition=%wide.region_4.5_spmd, body=%wide.region_1.4_spmd.sunk | while | flops 4388810752 | bytes 118582488 | solution.py:53
  1029.1 15.9 fusion.154
  1045.0 15.2 fusion.155
  1077.7 15.9 fusion.154
  1093.6 15.2 fusion.155
  1126.3 15.9 fusion.154
  1142.2 15.2 fusion.155
  1175.0 15.9 fusion.154
  1223.6 15.9 fusion.154
  1272.3 15.9 fusion.154
  1320.9 15.9 fusion.154
  1369.6 15.9 fusion.154
  1415.7 41.9 %bitcast_convert_fusion = bf16[4096,4096]{1,0:T(8,128)(2,1)} fusion(bf16[8,128,4096]{2,1,0:T(8,128)(2,1)} %param.19, bf16[2048,8,128]{2,0,1:T(8,128)(2,1)} %bitcast.161, bf16[2048,8,128]{2,0,1:T(8,128)(2,1)} %bitcast.160), kind=kOutput, calls=%fused_computation.59 | convolution fusion | flops 34393292800 | bytes 50331648 | tf_op jit(solution)/shard_map/shk,hkd->sd/dot_general | solution.py:88
  1458.3 225.5 %reduce-scatter.7.cloned.1.call-done = bf16[1024,4096]{1,0:T(8,128)(2,1)} async-done(((bf16[4096,4096]{1,0:T(8,128)(2,1)}), bf16[1024,4096]{1,0:T(8,128)(2,1)}) %reduce-scatter.7.cloned.1.call-update) | async-done | bytes 8388624
  1703.4 199.5 %all-gather.9.cloned.1.call-done = bf16[4096,4096]{1,0:T(8,128)(2,1)} async-done(((bf16[1024,4096]{1,0:T(8,128)(2,1)}), bf16[4096,4096]{1,0:T(8,128)(2,1)}) %all-gather.9.cloned.1.call-update) | async-done | bytes 33554448 | tf_op jit(solution)/shard_map/all_gather | solution.py:91
  1902.8 114.8 %fusion.126 = f32[4096,3072]{1,0:T(8,128)} fusion(bf16[4096,4096]{1,0:T(8,128)(2,1)} %all-gather.9.cloned.1.call-done, bf16[4096,3072]{1,0:T(8,128)(2,1)} %param.22), kind=kOutput, calls=%fused_computation.134 | convolution fusion | flops 103079215104 | bytes 109051904 | tf_op jit(solution)/shard_map/dot_general | solution.py:93
  2017.6 114.9 %fusion.125 = f32[4096,3072]{1,0:T(8,128)} fusion(bf16[4096,4096]{1,0:T(8,128)(2,1)} %all-gather.9.cloned.1.call-done, bf16[4096,3072]{1,0:T(8,128)(2,1)} %param.21), kind=kOutput, calls=%fused_computation.133 | convolution fusion | flops 103079215104 | bytes 109051904 | tf_op jit(solution)/shard_map/dot_general | solution.py:92
  2132.5 120.5 %convolution_convert_fusion = bf16[4096,4096]{1,0:T(8,128)(2,1)} fusion(bf16[3072,4096]{1,0:T(8,128)(2,1)} %param.23, f32[4096,3072]{1,0:T(8,128)} %fusion.126, f32[4096,3072]{1,0:T(8,128)} %fusion.125), kind=kOutput, calls=%fused_computation.63 | convolution fusion | flops 103171489792 | bytes 159383552 | tf_op jit(solution)/shard_map/dot_general | solution.py:95
  2253.1 226.2 %reduce-scatter.9.cloned.1.call-done = bf16[1024,4096]{1,0:T(8,128)(2,1)} async-done(((bf16[4096,4096]{1,0:T(8,128)(2,1)}), bf16[1024,4096]{1,0:T(8,128)(2,1)}) %reduce-scatter.9.cloned.1.call-update) | async-done | bytes 8388624
  (159 shorter events, 388.2 us)
Async XLA Ops:
  6.5 218.1 %copy-start = (bf16[4096,2,128]{2,1,0:T(2,128)(2,1)S(1)}, bf16[4096,2,128]{2,1,0:T(2,128)(2,1)}, u32[]{:S(2)}) copy-start(bf16[4096,2,128]{2,1,0:T(2,128)(2,1)} %param.18) | copy-start | bytes 6291460
  6.5 5.2 copy-start.7
  6.5 218.1 %all-gather.7.cloned.1.call-start = ((), (), s32[]{:S(2)}) async-start(), calls=%async_computation.2 | async-start | bytes 41943040 | tf_op jit(solution)/shard_map/all_gather | solution.py:68
  22.3 312.7 %all-gather.13.cloned.1.call-start = ((), (), s32[]{:S(2)}) async-start(), calls=%async_computation.5 | async-start | bytes 6291456 | tf_op jit(solution)/shard_map/all_gather | solution.py:76
  241.5 110.1 %all-gather.11.cloned.1.call-start = ((), (), s32[]{:S(2)}) async-start(), calls=%async_computation.4 | async-start | bytes 6291456 | tf_op jit(solution)/shard_map/all_gather | solution.py:75
  257.8 1.6 copy-start.2
  257.8 2.2 copy-start.3
  262.6 1421.2 %reduce-scatter.7.cloned.1.call-start = ((), (), s32[]{:S(2)}) async-start(), calls=%async_computation.6 | async-start | bytes 41943040
  312.5 6.5 copy-start.4
  375.8 650.8 %copy-start.6 = (s32[2,2048]{1,0:T(2,128)S(1)}, s32[2,2048]{1,0:T(2,128)}, u32[]{:S(2)}) copy-start(s32[2,2048]{1,0:T(2,128)} %compare_select_fusion) | copy-start | bytes 49156
  1045.0 15.2 copy-start.5
  1093.6 15.2 copy-start.5
  1142.2 15.2 copy-start.5
  1190.9 15.2 copy-start.5
  1239.5 15.2 copy-start.5
  1288.2 15.2 copy-start.5
  1336.8 15.2 copy-start.5
  1385.5 15.2 copy-start.5
  1457.6 0.7 copy-start.8
  1457.6 445.2 %all-gather.9.cloned.1.call-start = ((), (), s32[]{:S(2)}) async-start(), calls=%async_computation.3 | async-start | bytes 41943040 | tf_op jit(solution)/shard_map/all_gather | solution.py:91
  1703.3 776.0 %reduce-scatter.9.cloned.1.call-start = ((), (), s32[]{:S(2)}) async-start(), calls=%async_computation.7 | async-start | bytes 41943040
  2479.3 12.9 copy-start.1
Sparse Core Ops, SparseCore 0:
  22.5 202.1 all-gather.6
  241.6 54.1 all-gather.12
  297.4 54.1 all-gather.10
  1457.8 226.0 reduce-scatter.6
  1703.4 199.3 all-gather.8
  2253.2 226.0 reduce-scatter.8
where the time goes:
time: 2510 us; the launch traced here: 2500 us
  matrix products  1160 us (46%)
  waiting for transfers between devices  839 us (33%)
  other arithmetic  396 us (16%)
  local copies, waits for them, and re-layouts  76.4 us (3%)
    unnamed x8, waiting for transfers between devices  452 us
    dot_general x16, matrix products, one_tile(): jnp.einsum('qgrd,kgd->gqrk', q_tile, keys, preferred_element_type=jnp.flo...  353 us
    dot_general x16, matrix products, one_tile(): jnp.einsum('gqrk,kgd->gqrd', weights.astype(jnp.bfloat16), values, prefer...  342 us
    reduce_sum x16, other arithmetic, one_tile(): row_sum = jnp.sum(weights, axis=-1, keepdims=True)  294 us
    all_gather x1, waiting for transfers between devices, local_layer(): lax.all_gather(rms_norm(resid_rows, g_mlp), 'tp', axis=0, tiled=True)  199 us
    all_gather x1, waiting for transfers between devices, local_layer(): normed = lax.all_gather(rms_norm(x_rows, g_attn), 'tp', axis=0, tiled=True)  174 us
    dot_general x1, matrix products, local_layer(): jnp.dot(hidden, w_down, preferred_element_type=jnp.float32)  121 us
    dot_general x1, matrix products, local_layer(): gate_proj = jnp.dot(normed_mlp, w_gate, preferred_element_type=jnp.float32)  115 us
  transfers between devices with their start and end apart: 6, of which 5 were waited for; matrix products, arithmetic and copies ran while one was open for 5% of the time, Pallas kernels for 0%

commit v1 on v0

v1 whole, which is shorter than its diff:
```python
import functools
import math
import jax
import jax.numpy as jnp
from jax import lax
from jax.experimental import pallas as pl
from jax.experimental.pallas import tpu as pltpu
from jax.sharding import PartitionSpec as P

NORM_EPS = 1e-5
ROPE_THETA = 500000.0
HD = 128
NEG = -1e30
LOG2E = math.log2(math.e)
DN = (((1,), (0,)), ((), ()))
MIB = 1 << 20


def rms_norm(rows_in, gain_vec):
    rows_f32 = rows_in.astype(jnp.float32)
    mean_sq = jnp.mean(rows_f32 * rows_f32, axis=-1, keepdims=True)
    return (rows_f32 * lax.rsqrt(mean_sq + NORM_EPS) * gain_vec.astype(jnp.float32)).astype(jnp.bfloat16)


def rope_tables(positions):
    half = HD // 2
    inv_freq = ROPE_THETA ** (-2.0 * jnp.arange(half, dtype=jnp.float32) / HD)
    angles = positions.astype(jnp.float32)[:, None] * inv_freq[None, :]
    cos, sin = jnp.cos(angles), jnp.sin(angles)
    return jnp.concatenate([cos, cos], axis=-1), jnp.concatenate([-sin, sin], axis=-1)


def stored_positions(row_ids, piece_len, cp_size):
    owner_cp = row_ids // (2 * piece_len)
    within = row_ids % (2 * piece_len)
    return jnp.where(within < piece_len, owner_cp * piece_len + within,
                     (2 * cp_size - 1 - owner_cp) * piece_len + within - piece_len)


def qkv_kernel(a_ref, wq_ref, wk_ref, wv_ref, cos_ref, sin_ref, q_ref, k_ref, vt_ref):
    a = a_ref[...]
    cos, sin = cos_ref[...], sin_ref[...]

    def rope(val):
        f = val.astype(jnp.bfloat16).astype(jnp.float32)
        return (f * cos + pltpu.roll(f, HD // 2, 1) * sin).astype(jnp.bfloat16)

    nq = wq_ref.shape[1]
    for n in range(0, nq, 256):
        r = jnp.dot(a, wq_ref[:, n:n + 256], preferred_element_type=jnp.float32)
        q_ref[:, n:n + HD] = rope(r[:, :HD])
        q_ref[:, n + HD:n + 256] = rope(r[:, HD:])
    r = jnp.dot(a, wk_ref[...], preferred_element_type=jnp.float32)
    for n in range(0, wk_ref.shape[1], HD):
        k_ref[:, n:n + HD] = rope(r[:, n:n + HD])
    r = jnp.dot(a, wv_ref[...], preferred_element_type=jnp.float32)
    for n in range(0, wv_ref.shape[1], HD):
        vt_ref[n:n + HD, :] = r[:, n:n + HD].T.astype(jnp.bfloat16)


def qkv(a, wq, wk, wv, cos, sin, tile=256):
    rows, dim = a.shape
    nq, nk = wq.shape[1], wk.shape[1]
    whole = lambda shape: pl.BlockSpec(shape, lambda i: (0, 0), pipeline_mode=pl.Buffered(1))
    return pl.pallas_call(
        qkv_kernel,
        grid=(rows // tile,),
        in_specs=[pl.BlockSpec((tile, dim), lambda i: (i, 0)), whole((dim, nq)), whole((dim, nk)), whole((dim, nk)),
                  pl.BlockSpec((tile, HD), lambda i: (i, 0)), pl.BlockSpec((tile, HD), lambda i: (i, 0))],
        out_specs=[pl.BlockSpec((tile, nq), lambda i: (i, 0)), pl.BlockSpec((tile, nk), lambda i: (i, 0)),
                   pl.BlockSpec((nk, tile), lambda i: (0, i))],
        out_shape=[jax.ShapeDtypeStruct((rows, nq), jnp.bfloat16), jax.ShapeDtypeStruct((rows, nk), jnp.bfloat16),
                   jax.ShapeDtypeStruct((nk, rows), jnp.bfloat16)],
        name="qkv",
        cost_estimate=pl.CostEstimate(flops=2 * rows * dim * (nq + 2 * nk), transcendentals=0,
                                      bytes_accessed=2 * (rows * dim + dim * (nq + 2 * nk) + rows * (nq + 2 * nk))),
        compiler_params=pltpu.CompilerParams(dimension_semantics=("arbitrary",), vmem_limit_bytes=56 * MIB),
    )(a, wq, wk, wv, cos, sin)


def flash_kernel(qpos_ref, order_ref, q_ref, k_ref, vt_ref, o_ref,
                 qt_scr, s_scr, mb_scr, acc_scr, m_scr, l_scr, *, T, B, G, D, piece):
    p0 = qpos_ref[pl.program_id(1)]
    c = (HD ** -0.5) * LOG2E
    ppb = piece // B

    for h in range(G):
        qt_scr[h] = q_ref[:, h * HD:(h + 1) * HD].astype(jnp.float32).T.astype(jnp.bfloat16)
    m_scr[...] = jnp.full_like(m_scr, NEG)
    l_scr[...] = jnp.zeros_like(l_scr)
    acc_scr[...] = jnp.zeros_like(acc_scr)

    def off(b):
        st = order_ref[lax.div(b, ppb)]
        return lax.div(st, 2), pl.multiple_of(lax.rem(st, 2) * piece + lax.rem(b, ppb) * B, B)

    def put(s, slot, mask):
        if mask is not None:
            s = jnp.where(mask, s, NEG)
        s_scr[slot] = s
        mb = jnp.max(s.reshape(B // 8, 8, T), axis=0)
        for r in (4, 2, 1):
            mb = jnp.maximum(mb, pltpu.roll(mb, r, 0))
        mb_scr[slot] = mb

    def stage_a(at, h, mask=None):
        kb = k_ref[at[0], pl.ds(at[1], B), :]
        put(lax.dot_general(kb, qt_scr[h], DN, preferred_element_type=jnp.float32), h, mask)

    def stage_b(at, h):
        m_prev = m_scr[h]
        m_new = jnp.maximum(m_prev, mb_scr[h])
        m_scr[h] = m_new
        m_c = m_new * c
        p = jnp.exp2(s_scr[h].reshape(B // 8, 8, T) * c - m_c[None])
        alpha = jnp.exp2(m_prev * c - m_c)
        l_scr[h] = l_scr[h] * alpha + jnp.sum(p, axis=0)
        vb = vt_ref[at[0], :, pl.ds(at[1], B)]
        pv = lax.dot_general(vb, p.reshape(B, T).astype(jnp.bfloat16), DN, preferred_element_type=jnp.float32)
        acc_scr[h] = (acc_scr[h].reshape(HD // 8, 8, T) * alpha[None]).reshape(HD, T) + pv

    nfull = lax.div(p0, B)
    for h in range(D):
        stage_a(off(0), h)

    def body(j, carry):
        cur, nxt = off(j), off(j + 1)
        for h in range(G):
            a = h + D
            stage_a(cur if a < G else nxt, a % G)
            stage_b(cur, h)
        return carry

    lax.fori_loop(0, nfull, body, 0)

    cur = off(nfull)
    kp = nfull * B + lax.broadcasted_iota(jnp.int32, (B, T), 0)
    qp = p0 + lax.broadcasted_iota(jnp.int32, (B, T), 1)
    mask = kp <= qp
    for h in range(D):
        put(s_scr[h], h, mask)
    for h in range(G):
        if h + D < G:
            stage_a(cur, h + D, mask)
        stage_b(cur, h)
    for h in range(G):
        l = jnp.sum(l_scr[h], axis=0, keepdims=True)
        o_ref[:, h * HD:(h + 1) * HD] = (acc_scr[h] / l).T.astype(jnp.bfloat16)


def flash(qpos, order, q, k, vt, *, piece, T=256, B=512, D=3):
    rows, nq = q.shape
    cps, seq, nk = k.shape
    n_kv = nk // HD
    G = nq // nk
    keys = cps * seq
    return pl.pallas_call(
        functools.partial(flash_kernel, T=T, B=B, G=G, D=D, piece=piece),
        grid_spec=pltpu.PrefetchScalarGridSpec(
            num_scalar_prefetch=2, grid=(n_kv, rows // T),
            in_specs=[pl.BlockSpec((T, G * HD), lambda g, i, *_: (i, g)),
                      pl.BlockSpec((cps, seq, HD), lambda g, i, *_: (0, 0, g)),
                      pl.BlockSpec((cps, HD, seq), lambda g, i, *_: (0, g, 0))],
            out_specs=pl.BlockSpec((T, G * HD), lambda g, i, *_: (i, g)),
            scratch_shapes=[pltpu.VMEM((G, HD, T), jnp.bfloat16),
                            pltpu.VMEM((G, B, T), jnp.float32),
                            pltpu.VMEM((G, 8, T), jnp.float32),
                            pltpu.VMEM((G, HD, T), jnp.float32),
                            pltpu.VMEM((G, 8, T), jnp.float32),
                            pltpu.VMEM((G, 8, T), jnp.float32)]),
        out_shape=jax.ShapeDtypeStruct((rows, nq), jnp.bfloat16),
        name="flash",
        cost_estimate=pl.CostEstimate(flops=2 * rows * keys * nq, transcendentals=rows * keys * nq // HD // 2,
                                      bytes_accessed=4 * rows * nq + 4 * keys * nk),
        compiler_params=pltpu.CompilerParams(dimension_semantics=("arbitrary", "arbitrary"), vmem_limit_bytes=56 * MIB),
    )(qpos, order, q, k, vt)


def solution(mesh):
    cp_size = mesh.shape['cp']
    row_spec = P('dp', ('cp', 'tp'), None)
    head_cols = P(None, 'tp', None)

    def local_layer(x, g_attn, w_q, w_k, w_v, w_o, g_mlp, w_gate, w_up, w_down):
        x_rows = x[0]
        dim = w_q.shape[0]
        cp_index = lax.axis_index('cp')
        normed = lax.all_gather(rms_norm(x_rows, g_attn), 'tp', axis=0, tiled=True)
        seq_local = normed.shape[0]
        piece_len = seq_local // 2
        positions = stored_positions(cp_index * seq_local + jnp.arange(seq_local, dtype=jnp.int32), piece_len, cp_size)
        cos, sin = rope_tables(positions)
        q, k, vt = qkv(normed, w_q.reshape(dim, -1), w_k.reshape(dim, -1), w_v.reshape(dim, -1), cos, sin)
        k_seq = lax.all_gather(k, 'cp', axis=0, tiled=False)
        vt_seq = lax.all_gather(vt, 'cp', axis=0, tiled=False)
        order = jnp.array([2 * p if p < cp_size else 2 * (2 * cp_size - 1 - p) + 1 for p in range(2 * cp_size)], jnp.int32)
        attn_out = flash(positions[::256], order, q, k_seq, vt_seq, piece=piece_len)
        attn_part = jnp.dot(attn_out, w_o.reshape(-1, dim), preferred_element_type=jnp.float32).astype(jnp.bfloat16)
        attn_rows = lax.psum_scatter(attn_part, 'tp', scatter_dimension=0, tiled=True)
        resid_rows = (x_rows.astype(jnp.float32) + attn_rows.astype(jnp.float32)).astype(jnp.bfloat16)
        normed_mlp = lax.all_gather(rms_norm(resid_rows, g_mlp), 'tp', axis=0, tiled=True)
        gate_proj = jnp.dot(normed_mlp, w_gate, preferred_element_type=jnp.float32)
        up_proj = jnp.dot(normed_mlp, w_up, preferred_element_type=jnp.float32)
        hidden = (jax.nn.silu(gate_proj) * up_proj).astype(jnp.bfloat16)
        down_part = jnp.dot(hidden, w_down, preferred_element_type=jnp.float32).astype(jnp.bfloat16)
        down_rows = lax.psum_scatter(down_part, 'tp', scatter_dimension=0, tiled=True)
        z_rows = (resid_rows.astype(jnp.float32) + down_rows.astype(jnp.float32)).astype(jnp.bfloat16)
        return z_rows[None]

    return jax.shard_map(local_layer, mesh=mesh,
                         in_specs=(row_spec, P(), head_cols, head_cols, head_cols, P('tp', None, None),
                                   P(), P(None, 'tp'), P(None, 'tp'), P('tp', None)),
                         out_specs=row_spec, check_vma=False)
```

time: 2510 us -> 1690 us (0.67)
  matrix products: 1160 us -> 393 us
  other arithmetic: 396 us -> 59.3 us
  Pallas kernels: 0 us -> 266 us
  waiting for transfers between devices: 839 us -> 940 us
  local copies, waits for them, and re-layouts: 76.4 us -> 12.7 us
    dot_general x34 -> x1, matrix products: 754 us -> 43 us  [local_layer(): jnp.dot(attn_out, w_o.reshape(-1, dim), preferred_element_type=jnp.float32)]
    reduce_sum x16 -> x0, other arithmetic: 294 us -> none  [one_tile(): row_sum = jnp.sum(weights, axis=-1, keepdims=True)]
    pallas_call x0 -> x2, Pallas kernels: none -> 266 us  [the longest x1 202 us: flash(): pl.pallas_call(functools.partial(flash_kernel, T=T, B=B, G=G, D=D, piece=...]
    all_gather x2, waiting for transfers between devices: 13.5 us -> 108 us  [the longest x1 55.7 us: local_layer(): vt_seq = lax.all_gather(vt, 'cp', axis=0, tiled=False)]
    unnamed x2 -> x0, matrix products: 58.9 us -> none
  transfers between devices with their start and end apart: 6 -> 6, of which waited for: 5 -> 6; matrix products, arithmetic and copies ran while one was open for 5% -> 1% of each run, Pallas kernels for 0% -> 0%
where the time goes in v1:
time: 1690 us
  waiting for transfers between devices  940 us (56%)
  matrix products  393 us (23%)
  Pallas kernels  266 us (16%)
  other arithmetic  59.3 us (4%)
    unnamed x8, waiting for transfers between devices  452 us
    pallas_call x1, Pallas kernels, flash(): pl.pallas_call(functools.partial(flash_kernel, T=T, B=B, G=G, D=D, piece=...  202 us
    all_gather x1, waiting for transfers between devices, local_layer(): lax.all_gather(rms_norm(resid_rows, g_mlp), 'tp', axis=0, tiled=True)  199 us
    all_gather x1, waiting for transfers between devices, local_layer(): normed = lax.all_gather(rms_norm(x_rows, g_attn), 'tp', axis=0, tiled=True)  179 us
    dot_general x1, matrix products, local_layer(): jnp.dot(hidden, w_down, preferred_element_type=jnp.float32)  121 us
    dot_general x1, matrix products, local_layer(): gate_proj = jnp.dot(normed_mlp, w_gate, preferred_element_type=jnp.float32)  115 us
    dot_general x1, matrix products, local_layer(): up_proj = jnp.dot(normed_mlp, w_up, preferred_element_type=jnp.float32)  115 us
    pallas_call x1, Pallas kernels, qkv(): pl.pallas_call(qkv_kernel, grid=(rows // tile,), in_specs=[pl.BlockSpec((...  63.8 us
  transfers between devices with their start and end apart: 6, of which 6 were waited for; matrix products, arithmetic and copies ran while one was open for 1% of the time, Pallas kernels for 0%

profile of v1, /device:TPU:0, one launch (start us, length us, event | category | flops | bytes accessed | tf_op | source)
XLA Modules:
  0.0 1685.6 jit_solution(9230783659908233472)
XLA Ops:
  6.5 0.0 all-gather.7.cloned.1.call-start
  6.5 5.1 fusion.4
  11.6 0.7 convert_element_type.53
  12.3 10.5 fusion.6
  22.8 0.0 all-gather.7.cloned.1.call-update
  22.9 0.6 all-gather.11.cloned.1.call-start
  23.4 0.0 copy-start
  23.4 8.9 copy.18
  32.3 0.0 copy-start.1
  32.4 7.5 fusion.9
  39.9 3.2 pad_maximum_fusion
  43.1 0.0 copy-done
  43.1 0.0 copy-done.1
  43.1 2.7 copy_bitcast_fusion.1
  45.8 179.4 %all-gather.7.cloned.1.call-done.a_ref = bf16[4096,4096]{1,0:T(8,128)(2,1)} async-done(((bf16[1024,4096]{1,0:T(8,128)(2,1)}), bf16[4096,4096]{1,0:T(8,128)(2,1)}) %all-gather.7.cloned.1.call-update) | async-done | bytes 33554448 | tf_op jit(solution)/shard_map/all_gather | solution.py:188
  225.2 63.8 %qkv.1 = (bf16[4096,1024]{1,0:T(8,128)(2,1)}, bf16[4096,256]{1,0:T(8,128)(2,1)}, bf16[256,4096]{1,0:T(8,128)(2,1)}) custom-call(bf16[4096,4096]{1,0:T(8,128)(2,1)} %all-gather.7.cloned.1.call-done.a_ref, bf16[4096,1024]{1,0:T(8,128)(2,1)} %bitcast.36, bf16[4096,256]{1,0:T(8,128)(2,1)} %get-tuple-element.17.wk_ref, ...), custom_call_target="tpu_custom_call" | custom-call | flops 51539607552 | bytes 58720256 | tf_op jit(solution)/shard_map/qkv/pallas_call | solution.py:65
  289.0 0.0 all-gather.11.cloned.1.call-update
  289.1 0.0 all-gather.13.cloned.1.call-start
  289.1 0.7 all-gather.13.cloned.1.call-update
  289.8 0.2 reduce-scatter.7.cloned.1.call-start
  290.1 0.7 slice.3.qpos_ref
  290.7 52.7 %all-gather.11.cloned.1.call-done = bf16[8192,256]{1,0:T(8,128)(2,1)} async-done(((bf16[4096,256]{1,0:T(8,128)(2,1)}), bf16[8192,256]{1,0:T(8,128)(2,1)}) %all-gather.11.cloned.1.call-update) | async-done | bytes 4194320 | tf_op jit(solution)/shard_map/all_gather | solution.py:194
  343.4 55.7 %all-gather.13.cloned.1.call-done = bf16[512,4096]{1,0:T(8,128)(2,1)} async-done(((bf16[256,4096]{1,0:T(8,128)(2,1)}), bf16[512,4096]{1,0:T(8,128)(2,1)}) %all-gather.13.cloned.1.call-update) | async-done | bytes 4194320 | tf_op jit(solution)/shard_map/all_gather | solution.py:195
  399.1 201.9 %flash.1 = bf16[4096,1024]{1,0:T(8,128)(2,1)} custom-call(s32[16]{0:T(128)} %slice.3.qpos_ref, s32[4]{0:T(128)} %constant.62.clone.order_ref, bf16[4096,1024]{1,0:T(8,128)(2,1)} %get-tuple-element.8.q_ref, bf16[2,4096,256]{2,1,0:T(8,128)(2,1)} %bitcast.40, bf16[2,256,4096]{2,1,0:T(8,128)(2,1)} %bitcast.41), custom_call_target="tpu_custom_call" | custom-call | flops 68719476736 | bytes 25165824 | tf_op jit(solution)/shard_map/flash/pallas_call | solution.py:157
  601.0 43.0 %convolution_convert_fusion.1 = bf16[4096,4096]{1,0:T(8,128)(2,1)} fusion(bf16[4096,1024]{1,0:T(8,128)(2,1)} %flash.1, bf16[1024,4096]{1,0:T(8,128)(2,1)} %bitcast.39), kind=kOutput, calls=%fused_computation.2 | convolution fusion | flops 34376515584 | bytes 50331648 | tf_op jit(solution)/shard_map/dot_general | solution.py:198
  644.0 0.0 copy-start.2
  644.0 0.0 reduce-scatter.7.cloned.1.call-update
  644.1 0.3 all-gather.9.cloned.1.call-start
  644.3 0.4 copy-done.2
  644.7 225.5 %reduce-scatter.7.cloned.1.call-done = bf16[1024,4096]{1,0:T(8,128)(2,1)} async-done(((bf16[4096,4096]{1,0:T(8,128)(2,1)}), bf16[1024,4096]{1,0:T(8,128)(2,1)}) %reduce-scatter.7.cloned.1.call-update) | async-done | bytes 8388624
  870.3 8.5 fusion
  878.8 10.9 fusion.2
  889.7 0.0 all-gather.9.cloned.1.call-update
  889.8 0.0 reduce-scatter.9.cloned.1.call-start
  889.8 199.4 %all-gather.9.cloned.1.call-done = bf16[4096,4096]{1,0:T(8,128)(2,1)} async-done(((bf16[1024,4096]{1,0:T(8,128)(2,1)}), bf16[4096,4096]{1,0:T(8,128)(2,1)}) %all-gather.9.cloned.1.call-update) | async-done | bytes 33554448 | tf_op jit(solution)/shard_map/all_gather | solution.py:201
  1089.3 114.7 %fusion.18 = f32[4096,3072]{1,0:T(8,128)} fusion(bf16[4096,4096]{1,0:T(8,128)(2,1)} %all-gather.9.cloned.1.call-done, bf16[4096,3072]{1,0:T(8,128)(2,1)} %param.19), kind=kOutput, calls=%fused_computation.45 | convolution fusion | flops 103079215104 | bytes 109051904 | tf_op jit(solution)/shard_map/dot_general | solution.py:203
  1203.9 114.9 %fusion.17 = f32[4096,3072]{1,0:T(8,128)} fusion(bf16[4096,4096]{1,0:T(8,128)(2,1)} %all-gather.9.cloned.1.call-done, bf16[4096,3072]{1,0:T(8,128)(2,1)} %param.18), kind=kOutput, calls=%fused_computation.44 | convolution fusion | flops 103079215104 | bytes 109051904 | tf_op jit(solution)/shard_map/dot_general | solution.py:202
  1318.8 120.5 %convolution_convert_fusion = bf16[4096,4096]{1,0:T(8,128)(2,1)} fusion(bf16[3072,4096]{1,0:T(8,128)(2,1)} %param.20, f32[4096,3072]{1,0:T(8,128)} %fusion.18, f32[4096,3072]{1,0:T(8,128)} %fusion.17), kind=kOutput, calls=%fused_computation.1 | convolution fusion | flops 103171489792 | bytes 159383552 | tf_op jit(solution)/shard_map/dot_general | solution.py:205
  1439.3 0.0 reduce-scatter.9.cloned.1.call-update
  1439.3 226.2 %reduce-scatter.9.cloned.1.call-done = bf16[1024,4096]{1,0:T(8,128)(2,1)} async-done(((bf16[4096,4096]{1,0:T(8,128)(2,1)}), bf16[1024,4096]{1,0:T(8,128)(2,1)}) %reduce-scatter.9.cloned.1.call-update) | async-done | bytes 8388624
  1665.5 12.8 fusion.8
  (6 shorter events, 0.1 us)
Async XLA Ops:
  6.5 218.7 %all-gather.7.cloned.1.call-start = ((), (), s32[]{:S(2)}) async-start(), calls=%async_computation.2 | async-start | bytes 41943040 | tf_op jit(solution)/shard_map/all_gather | solution.py:188
  22.9 320.5 %all-gather.11.cloned.1.call-start = ((), (), s32[]{:S(2)}) async-start(), calls=%async_computation.4 | async-start | bytes 6291456 | tf_op jit(solution)/shard_map/all_gather | solution.py:194
  23.4 19.7 %copy-start = (bf16[4096,2,128]{2,1,0:T(2,128)(2,1)S(1)}, bf16[4096,2,128]{2,1,0:T(2,128)(2,1)}, u32[]{:S(2)}) copy-start(bf16[4096,2,128]{2,1,0:T(2,128)(2,1)} %param.15) | copy-start | bytes 6291460
  32.3 10.7 copy-start.1
  289.1 110.1 %all-gather.13.cloned.1.call-start = ((), (), s32[]{:S(2)}) async-start(), calls=%async_computation.5 | async-start | bytes 6291456 | tf_op jit(solution)/shard_map/all_gather | solution.py:195
  289.8 580.5 %reduce-scatter.7.cloned.1.call-start = ((), (), s32[]{:S(2)}) async-start(), calls=%async_computation.6 | async-start | bytes 41943040
  644.0 0.7 copy-start.2
  644.1 445.2 %all-gather.9.cloned.1.call-start = ((), (), s32[]{:S(2)}) async-start(), calls=%async_computation.3 | async-start | bytes 41943040 | tf_op jit(solution)/shard_map/all_gather | solution.py:201
  889.8 775.7 %reduce-scatter.9.cloned.1.call-start = ((), (), s32[]{:S(2)}) async-start(), calls=%async_computation.7 | async-start | bytes 41943040
Sparse Core Ops, SparseCore 0:
  23.0 202.1 all-gather.6
  289.2 54.1 all-gather.10
  344.9 54.1 all-gather.12
  644.2 226.0 reduce-scatter.6
  889.9 199.3 all-gather.8
  1439.4 225.9 reduce-scatter.8

commit v2 on v0

v2 whole, which is shorter than its diff:
```python
import functools
import math
import jax
import jax.numpy as jnp
import numpy as np
from jax import lax
from jax.experimental import pallas as pl
from jax.experimental.pallas import tpu as pltpu
from jax.sharding import PartitionSpec as P

NORM_EPS = 1e-5
ROPE_THETA = 500000.0
HD = 128
RUN = 256
NEG = -1e30
FAR = 1 << 29
LOG2E = math.log2(math.e)
DN = (((1,), (0,)), ((), ()))
MIB = 1 << 20
BF = jnp.bfloat16
F32 = jnp.float32
ANY = pl.BlockSpec(memory_space=pl.ANY)


def params(n, mib):
    return pltpu.CompilerParams(dimension_semantics=("arbitrary",) * n, vmem_limit_bytes=mib * MIB)


def rope_tables(positions):
    half = HD // 2
    inv_freq = ROPE_THETA ** (-2.0 * jnp.arange(half, dtype=F32) / HD)
    angles = positions.astype(F32)[..., None] * inv_freq
    cos, sin = jnp.cos(angles), jnp.sin(angles)
    return jnp.concatenate([cos, cos], axis=-1), jnp.concatenate([-sin, sin], axis=-1)


def norm_rows(rows, gain):
    f = rows.astype(F32)
    mean_sq = jnp.mean(f * f, axis=-1, keepdims=True)
    return (f * lax.rsqrt(mean_sq + NORM_EPS) * gain.astype(F32)).astype(BF)


def ordered(kernel, n_in, after):
    n = len(after)
    return lambda *refs: kernel(*refs[:n_in], *refs[n_in + n:])


def load_all(pairs, sem):
    copies = [pltpu.make_async_copy(src, dst, sem.at[i]) for i, (src, dst) in enumerate(pairs)]
    for cp in copies:
        cp.start()
    for cp in copies:
        cp.wait()


def norm_kernel(x_ref, g_ref, o_ref):
    o_ref[...] = norm_rows(x_ref[...], g_ref[...])


def norm_run(x_rows, gain, j, after=(), tile=128):
    dim = x_rows.shape[1]
    per = RUN // tile
    return pl.pallas_call(
        ordered(norm_kernel, 2, after), grid=(per,),
        in_specs=[pl.BlockSpec((tile, dim), lambda i: (j * per + i, 0)), pl.BlockSpec((1, dim), lambda i: (0, 0))]
        + [ANY] * len(after),
        out_specs=pl.BlockSpec((tile, dim), lambda i: (i, 0)),
        out_shape=jax.ShapeDtypeStruct((RUN, dim), BF),
        name="norm", compiler_params=params(1, 60),
        cost_estimate=pl.CostEstimate(flops=8 * RUN * dim, transcendentals=0, bytes_accessed=4 * RUN * dim),
    )(x_rows, gain, *after)


def qkv_kernel(*refs, n_in, nq):
    a_refs = refs[:n_in]
    w_ref, cos_ref, sin_ref, q_ref, kv_ref, a_scr, sem = refs[n_in:]
    n = pl.program_id(0)

    @pl.when(n == 0)
    def _():
        load_all([(r, a_scr.at[pl.ds(i * RUN, RUN), :]) for i, r in enumerate(a_refs)], sem)

    r = jnp.dot(a_scr[...], w_ref[...], preferred_element_type=F32)

    def rope(h):
        f = r[:, h * HD:(h + 1) * HD].astype(BF).astype(F32)
        cos, sin = cos_ref[...].reshape(n_in * RUN, HD), sin_ref[...].reshape(n_in * RUN, HD)
        return (f * cos + pltpu.roll(f, HD // 2, 1) * sin).astype(BF).reshape(n_in, RUN, HD)

    @pl.when(n < nq)
    def _():
        for h in range(2):
            q_ref[:, :, h * HD:(h + 1) * HD] = rope(h)

    @pl.when(n == nq)
    def _():
        for h in range(2):
            kv_ref[:, 0, :, h * HD:(h + 1) * HD] = rope(h)

    @pl.when(n == nq + 1)
    def _():
        for i in range(n_in):
            for h in range(2):
                kv_ref[i, 0, h * HD:(h + 1) * HD, :] = r[i * RUN:(i + 1) * RUN, h * HD:(h + 1) * HD].T.astype(BF)


def qkv(rows, w_all, cos, sin, first_run, after=()):
    n_in = len(rows)
    dim, cols = w_all.shape
    nq = cols // 256 - 2
    at = first_run // n_in
    tab = pl.BlockSpec((n_in, RUN, HD), lambda n: (at, 0, 0))
    return pl.pallas_call(
        ordered(functools.partial(qkv_kernel, n_in=n_in, nq=nq), n_in + 3, after),
        grid=(nq + 2,),
        in_specs=[ANY] * n_in + [pl.BlockSpec((dim, 256), lambda n: (0, n)), tab, tab] + [ANY] * len(after),
        out_specs=[pl.BlockSpec((n_in, RUN, 256), lambda n: (0, 0, jnp.minimum(n, nq - 1))),
                   pl.BlockSpec((n_in, 1, 256, 256), lambda n: (0, jnp.maximum(n - nq, 0), 0, 0))],
        out_shape=[jax.ShapeDtypeStruct((n_in, RUN, nq * 256), BF), jax.ShapeDtypeStruct((n_in, 2, 256, 256), BF)],
        scratch_shapes=[pltpu.VMEM((n_in * RUN, dim), BF), pltpu.SemaphoreType.DMA((n_in,))],
        name="qkv", compiler_params=params(1, 60),
        cost_estimate=pl.CostEstimate(flops=2 * n_in * RUN * dim * cols, transcendentals=0,
                                      bytes_accessed=2 * (n_in * RUN * dim + dim * cols + n_in * RUN * cols)),
    )(*rows, w_all, cos, sin, *after)


def flash_kernel(tab_ref, *refs, q_src, kv_src, n_q, n_kv, base, stride, G, D, n_out):
    qs, kvs = refs[:n_q], refs[n_q:n_q + n_kv]
    outs = refs[n_q + n_kv:n_q + n_kv + n_out]
    q_scr, kv_scr, qt_scr, s_scr, mb_scr, acc_scr, m_scr, l_scr, sem = refs[n_q + n_kv + n_out:]
    tile, g = pl.program_id(0), pl.program_id(1)
    T = RUN
    c = (HD ** -0.5) * LOG2E

    @pl.when((tile == 0) & (g == 0))
    def _():
        load_all([(qs[a].at[pl.ds(i, n)], q_scr.at[pl.ds(dst, n)]) for dst, (a, i, n) in q_src]
                 + [(kvs[a], kv_scr.at[pl.ds(dst, n)]) for a, (dst, n) in enumerate(kv_src)], sem)

    row = base + tile * stride
    npairs = tab_ref[row]
    qpos = tab_ref[row + 1]
    gcol = pl.multiple_of(g * HD, HD)

    for h in range(G):
        qh = q_scr[tile, :, pl.ds(pl.multiple_of((g * G + h) * HD, HD), HD)]
        qt_scr[h] = qh.astype(F32).T.astype(BF)
    m_scr[...] = jnp.full_like(m_scr, NEG)
    l_scr[...] = jnp.zeros_like(l_scr)
    acc_scr[...] = jnp.zeros_like(acc_scr)

    def pair(p):
        return tab_ref[row + 4 + 2 * p], tab_ref[row + 5 + 2 * p]

    def put(s, h):
        s_scr[h] = s
        mb = jnp.max(s.reshape(2 * RUN // 8, 8, T), axis=0)
        for r in (4, 2, 1):
            mb = jnp.maximum(mb, pltpu.roll(mb, r, 0))
        mb_scr[h] = mb

    def stage_a(pr, h, mask=None):
        s = jnp.concatenate([lax.dot_general(kv_scr[r, 0, :, pl.ds(gcol, HD)], qt_scr[h], DN, preferred_element_type=F32)
                             for r in pr], axis=0)
        put(s if mask is None else jnp.where(mask, s, NEG), h)

    def stage_b(pr, h):
        m_prev = m_scr[h]
        m_new = jnp.maximum(m_prev, mb_scr[h])
        m_scr[h] = m_new
        m_c = m_new * c
        p = jnp.exp2(s_scr[h].reshape(2 * RUN // 8, 8, T) * c - m_c[None])
        alpha = jnp.exp2(m_prev * c - m_c)
        l_scr[h] = l_scr[h] * alpha + jnp.sum(p, axis=0)
        pb = p.reshape(2 * RUN, T).astype(BF)
        pv = sum(lax.dot_general(kv_scr[r, 1, pl.ds(gcol, HD), :], pb[i * RUN:(i + 1) * RUN], DN, preferred_element_type=F32)
                 for i, r in enumerate(pr))
        acc_scr[h] = (acc_scr[h].reshape(HD // 8, 8, T) * alpha[None]).reshape(HD, T) + pv

    first = pair(0)
    for h in range(D):
        stage_a(first, h)

    def body(j, carry):
        cur, nxt = pair(j), pair(j + 1)
        for h in range(G):
            a = h + D
            stage_a(cur if a < G else nxt, a % G)
            stage_b(cur, h)
        return carry

    lax.fori_loop(0, npairs - 1, body, 0)

    last = pair(npairs - 1)
    key = lax.broadcasted_iota(jnp.int32, (RUN, T), 0)
    qry = lax.broadcasted_iota(jnp.int32, (RUN, T), 1) + qpos
    mask = jnp.concatenate([key + tab_ref[row + 2] <= qry, key + tab_ref[row + 3] <= qry], axis=0)
    for h in range(D):
        put(jnp.where(mask, s_scr[h], NEG), h)
    for h in range(G):
        if h + D < G:
            stage_a(last, h + D, mask)
        stage_b(last, h)
    for h in range(G):
        l = jnp.sum(l_scr[h], axis=0, keepdims=True)
        q_scr[tile, :, pl.ds(pl.multiple_of((g * G + h) * HD, HD), HD)] = (acc_scr[h] / l).T.astype(BF)
    for k in range(n_out):
        @pl.when(tile == k)
        def _():
            outs[k][...] = q_scr[k, :, pl.ds(pl.multiple_of(g * G * HD, G * HD), G * HD)]


def flash(tab, qs, q_src, kvs, kv_src, *, base, stride, work, after=(), D=3):
    nq = qs[0].shape[2]
    n_kv_heads = 2
    G = nq // HD // n_kv_heads
    n_tiles = 4
    n_runs = max(d + n for d, n in kv_src)

    def out_spec(k):
        return pl.BlockSpec((RUN, G * HD), lambda i, g, *_: (0, jnp.where(i < k, 0, jnp.where(i == k, g, n_kv_heads - 1))))

    return pl.pallas_call(
        ordered(functools.partial(flash_kernel, q_src=q_src, kv_src=kv_src, n_q=len(qs), n_kv=len(kvs), base=base,
                                  stride=stride, G=G, D=D, n_out=n_tiles), 1 + len(qs) + len(kvs), after),
        grid_spec=pltpu.PrefetchScalarGridSpec(
            num_scalar_prefetch=1, grid=(n_tiles, n_kv_heads),
            in_specs=[ANY] * (len(qs) + len(kvs) + len(after)),
            out_specs=[out_spec(k) for k in range(n_tiles)],
            scratch_shapes=[pltpu.VMEM((n_tiles, RUN, nq), BF),
                            pltpu.VMEM((n_runs, 2, 256, 256), BF),
                            pltpu.VMEM((G, HD, RUN), BF),
                            pltpu.VMEM((G, 2 * RUN, RUN), F32),
                            pltpu.VMEM((G, 8, RUN), F32),
                            pltpu.VMEM((G, HD, RUN), F32),
                            pltpu.VMEM((G, 8, RUN), F32),
                            pltpu.VMEM((G, 8, RUN), F32),
                            pltpu.SemaphoreType.DMA((len(q_src) + len(kv_src),))]),
        out_shape=[jax.ShapeDtypeStruct((RUN, nq), BF)] * n_tiles,
        name="flash", compiler_params=params(2, 60),
        cost_estimate=pl.CostEstimate(flops=8 * work * RUN * RUN * nq, transcendentals=work * RUN * RUN * nq // HD,
                                      bytes_accessed=n_runs * 2 * 256 * 256 * 2 + 4 * n_tiles * RUN * nq),
    )(tab, *qs, *kvs, *after)


def out_kernel(*refs, n_w):
    o_refs, w_refs = refs[:4], refs[4:4 + n_w]
    x_ref, g_ref, y_ref, b_ref, o_scr, sem = refs[4 + n_w:]
    n = pl.program_id(0)
    tn = w_refs[0].shape[1]
    width = o_refs[0].shape[1]
    half = width // 2

    @pl.when(n == 0)
    def _():
        mine = lax.axis_index('cp')
        pairs = [(o_refs[0], o_scr.at[:, pl.ds(0, width)]), (o_refs[1], o_scr.at[:, pl.ds(width, width)])]
        for k in range(2, 4):
            for i, part in enumerate((mine, 1 - mine)):
                pairs.append((o_refs[k].at[:, pl.ds(pl.multiple_of(part * half, half), half)],
                              o_scr.at[:, pl.ds(k * width + i * half, half)]))
        load_all(pairs, sem)

    acc, k0 = None, 0
    for w in w_refs:
        d = jnp.dot(o_scr[:, k0:k0 + w.shape[0]], w[...], preferred_element_type=F32)
        acc = d if acc is None else acc + d
        k0 += w.shape[0]
    cols = pl.ds(pl.multiple_of(n * tn, tn), tn)
    y_ref[:, cols] = (x_ref[:, cols].astype(F32) + acc.astype(BF).astype(F32)).astype(BF)

    @pl.when(n == pl.num_programs(0) - 1)
    def _():
        for i in range(0, RUN, 64):
            b_ref[i:i + 64, :] = norm_rows(y_ref[i:i + 64, :], g_ref[...])


def out_proj(os, ws, x_rows, gain, j, after=(), tn=512):
    dim = x_rows.shape[1]
    width = os[0].shape[1]
    whole = lambda s: pl.BlockSpec((RUN, dim), lambda n: (s, 0))
    return pl.pallas_call(
        ordered(functools.partial(out_kernel, n_w=len(ws)), 6 + len(ws), after),
        grid=(dim // tn,),
        in_specs=[ANY] * 4 + [pl.BlockSpec((w.shape[0], tn), lambda n: (0, n)) for w in ws]
        + [whole(j), pl.BlockSpec((1, dim), lambda n: (0, 0))] + [ANY] * len(after),
        out_specs=[whole(0), whole(0)],
        out_shape=[jax.ShapeDtypeStruct((RUN, dim), BF)] * 2,
        scratch_shapes=[pltpu.VMEM((RUN, 4 * width), BF), pltpu.SemaphoreType.DMA((6,))],
        name="outp", compiler_params=params(1, 60),
        cost_estimate=pl.CostEstimate(flops=8 * RUN * width * dim, transcendentals=0,
                                      bytes_accessed=8 * width * dim + 8 * RUN * dim),
    )(*os, *ws, x_rows, gain, *after)


def hidden_kernel(*refs, n_in):
    b_refs = refs[:n_in]
    wg_ref, wu_ref, u_ref, b_scr, sem = refs[n_in:]

    @pl.when(pl.program_id(0) == 0)
    def _():
        load_all([(r, b_scr.at[pl.ds(k * RUN, RUN), :]) for k, r in enumerate(b_refs)], sem)

    b = b_scr[...]
    gate = jnp.dot(b, wg_ref[...], preferred_element_type=F32)
    up = jnp.dot(b, wu_ref[...], preferred_element_type=F32)
    u_ref[...] = (jax.nn.silu(gate) * up).astype(BF)


def hidden(bs, wg, wu, after=(), tn=512):
    rows, dim = RUN * len(bs), bs[0].shape[1]
    ffn = wg.shape[1]
    cols = lambda i: (0, i)
    return pl.pallas_call(
        ordered(functools.partial(hidden_kernel, n_in=len(bs)), len(bs) + 2, after),
        grid=(ffn // tn,),
        in_specs=[ANY] * len(bs) + [pl.BlockSpec((dim, tn), cols)] * 2 + [ANY] * len(after),
        out_specs=pl.BlockSpec((rows, tn), cols),
        out_shape=jax.ShapeDtypeStruct((rows, ffn), BF),
        scratch_shapes=[pltpu.VMEM((rows, dim), BF), pltpu.SemaphoreType.DMA((len(bs),))],
        name="hidden", compiler_params=params(1, 60),
        cost_estimate=pl.CostEstimate(flops=4 * rows * dim * ffn, transcendentals=rows * ffn,
                                      bytes_accessed=4 * dim * ffn + 2 * rows * (dim + ffn)),
    )(*bs, wg, wu, *after)


def down_kernel(u_ref, w_ref, o_ref):
    o_ref[...] = jnp.dot(u_ref[...], w_ref[...], preferred_element_type=F32).astype(BF)


def down(u, wd, part, after=(), td=512):
    rows, ffn = u.shape[0] // 2, u.shape[1]
    dim = wd.shape[1]
    return pl.pallas_call(
        ordered(down_kernel, 2, after),
        grid=(dim // td,),
        in_specs=[pl.BlockSpec((rows, ffn), lambda i: (part, 0)), pl.BlockSpec((ffn, td), lambda i: (0, i))]
        + [ANY] * len(after),
        out_specs=pl.BlockSpec((rows, td), lambda i: (0, i)),
        out_shape=jax.ShapeDtypeStruct((rows, dim), BF),
        name="down", compiler_params=params(1, 60),
        cost_estimate=pl.CostEstimate(flops=2 * rows * dim * ffn, transcendentals=0,
                                      bytes_accessed=2 * dim * ffn + 2 * rows * (dim + ffn)),
    )(u, wd, *after)


def sum_kernel(*refs):
    p_ref, r_ref, t_ref, y_ref, z_ref = refs[-5:]
    total = p_ref[...].astype(F32) + r_ref[...].astype(F32) + t_ref[...].astype(F32)
    z_ref[...] = (y_ref[...].astype(F32) + total.astype(BF).astype(F32)).astype(BF)


def sum_run(z, keep, recv, far, y, j, n_runs, after=(), tile=64):
    dim = y.shape[1]
    per = RUN // tile
    spec = pl.BlockSpec((tile, dim), lambda i: (i, 0))
    prev = () if z is None else (z,)
    return pl.pallas_call(
        ordered(sum_kernel, len(prev) + 4, after), grid=(per,),
        in_specs=[ANY] * len(prev) + [spec] * 4 + [ANY] * len(after),
        out_specs=pl.BlockSpec((tile, dim), lambda i: (j * per + i, 0)),
        out_shape=jax.ShapeDtypeStruct((n_runs * RUN, dim), BF),
        input_output_aliases={0: 0} if prev else {},
        name="zsum", compiler_params=params(1, 60),
        cost_estimate=pl.CostEstimate(flops=6 * RUN * dim, transcendentals=0, bytes_accessed=10 * RUN * dim),
    )(*prev, keep, recv, far, y, *after)


def run_positions(xi, ci, y, cps, piece):
    def start(x, c):
        return (y if x == 0 else 2 * cps - 1 - y) * piece + c * (piece // 2)

    per = piece // 2 // RUN
    out = [start(xi, ci) + RUN * j for j in range(per)] + [start(xi, 1 - ci) + RUN * j for j in range(per)]
    for j in range(per):
        out += [start(1 - xi, ci) + RUN * j, start(1 - xi, 1 - ci) + RUN * j]
    return out


def work_tables(cps, piece):
    per = piece // 2 // RUN
    tabs, runs, work = [], [], []
    stride = 4 + 2 * (2 * per * 2 * cps // 2 + 1)
    for y in range(cps):
        for xi in range(2):
            for ci in range(2):
                mine = run_positions(xi, ci, y, cps, piece)
                pos = mine + run_positions(xi, ci, 1 - y, cps, piece)
                runs.append(mine)
                rows, amount = [], []
                for j in range(per):
                    for tile in (j, per + j, 2 * per + 2 * j, 2 * per + 2 * j + 1):
                        q = pos[tile]
                        ids = [r for r in range(len(pos)) if pos[r] < q] + [tile]
                        where = [pos[r] for r in ids]
                        if len(ids) % 2:
                            ids.append(tile)
                            where.append(FAR)
                        row = [len(ids) // 2, q, where[-2], where[-1]] + ids
                        rows.append(row + [0] * (stride - len(row)))
                        amount.append(len(ids))
                tabs.append(np.array(rows, np.int32).reshape(-1))
                work.append(amount)
    return np.stack(tabs), np.array(runs, np.int32), stride, np.array(work).reshape(len(tabs), per, 4).sum(-1).max(0)


def solution(mesh):
    cps = mesh.shape['cp']
    row_spec = P('dp', ('cp', 'tp'), None)
    head_cols = P(None, 'tp', None)
    n_tp = mesh.shape['tp']

    over_core, over_x, over_both = (('tp', [(t, t ^ k) for t in range(n_tp)]) for k in (1, 2, 3))
    over_y = ('cp', [(i, i ^ 1) for i in range(cps)])

    def layer(x, g_attn, w_q, w_k, w_v, w_o, g_mlp, w_gate, w_up, w_down):
        x_rows = x[0]
        dim = x_rows.shape[1]
        n_run = x_rows.shape[0] // RUN
        piece = 2 * x_rows.shape[0]
        t_id, y_id = lax.axis_index('tp'), lax.axis_index('cp')
        np_tab, np_runs, stride, work = work_tables(cps, piece)
        dev = y_id * n_tp + t_id
        tab = lax.dynamic_index_in_dim(jnp.asarray(np_tab), dev, 0, keepdims=False)
        run_pos = lax.dynamic_index_in_dim(jnp.asarray(np_runs), dev, 0, keepdims=False)

        def tied(v, *others):
            return lax.optimization_barrier((v, *others))[0]

        def send(axis_pairs, v):
            return lax.ppermute(v, *axis_pairs)

        ga, gm = g_attn.reshape(1, dim), g_mlp.reshape(1, dim)
        own = []
        for j in range(n_run):
            own.append(norm_run(x_rows, ga, j, after=own[-1:]))
        far = [send(over_x, own[j]) for j in range(n_run)]
        mate = [send(over_core, own[j]) for j in range(n_run)]

        w_all = jnp.concatenate([tied(w, own[-1]).reshape(dim, -1) for w in (w_q, w_k, w_v)], axis=1)
        cos, sin = rope_tables(tied(run_pos, own[-1])[:, None] + jnp.arange(RUN, dtype=jnp.int32)[None, :])

        q_own, kv_own = qkv(own, w_all, cos, sin, 0)
        q_mate, kv_mate = qkv(mate, w_all, cos, sin, n_run, after=(kv_own,))
        kvs = [kv_own, kv_mate]
        q_far = []
        for j in range(n_run):
            here = tied(far[j], kvs[-1])
            q, kv = qkv([here, send(over_core, here)], w_all, cos, sin, 2 * n_run + 2 * j,
                         after=(kvs[-1],))
            q_far.append(q)
            kvs.append(kv)
        gate, last = kvs[3], kvs[-1]
        kvs = kvs + [send(over_y, kv) for kv in kvs]
        kv_src, at = [], 0
        for kv in kvs:
            kv_src.append((at, kv.shape[0]))
            at += kv.shape[0]

        wo = w_o.reshape(-1, dim)
        half = wo.shape[0] // 2
        wo_gated = tied(wo, gate)
        wo_xa = send(over_x, lax.dynamic_slice_in_dim(wo_gated, y_id * half, half, axis=0))
        ws = [wo, send(over_core, wo_gated)]

        os, outs = [], []
        prev = last

        def attend(j):
            o_own, o_mate, o_far, o_fm = flash(
                tab, [q_own, q_mate, q_far[j]], [(0, (0, j, 1)), (1, (1, j, 1)), (2, (2, 0, 2))],
                kvs, kv_src, base=j * 4 * stride, stride=stride, work=int(work[j]), after=(prev,))
            os.append([o_own, send(over_core, o_mate), send(over_x, o_far), send(over_both, o_fm)])
            return o_own

        def project(j):
            y, b = out_proj(os[j], ws, x_rows, gm, j, after=(prev,))
            outs.append((y, b, send(over_x, b), send(over_core, b)))
            return b

        prev = attend(0)
        wo_a = tied(wo_xa, prev)
        wo_xb = send(over_y, wo_a)
        ws += [wo_a, None, send(over_core, wo_a), None]
        prev = attend(1)
        prev = attend(2)
        wo_b = tied(wo_xb, prev)
        ws[3], ws[5] = wo_b, send(over_core, wo_b)
        prev = project(0)
        prev = attend(3)

        z, pending, relay = None, None, {}

        def relay_b(j):
            here = tied(outs[j][2], prev)
            relay[j] = (here, send(over_core, here))

        relay_b(0)
        prev = project(1)
        for j in range(n_run):
            y, b, _, b_mate = outs[j]
            u = hidden([b, relay[j][0], b_mate, relay[j][1]], w_gate, w_up, after=(prev,))
            out = down(u, w_down, 1)
            recv = send(over_core, out)
            prev = out
            if j + 1 < n_run:
                relay_b(j + 1)
            keep = down(u, w_down, 0, after=(out,))
            prev = s_far = (keep[RUN:].astype(F32) + recv[RUN:].astype(F32)).astype(BF)
            got = send(over_x, s_far)
            if j + 2 < n_run:
                prev = project(j + 2)
            if pending is not None:
                prev = z = sum_run(z, *pending, j - 1, n_run, after=(prev,))
            pending = (keep, recv, got, y)
        z = sum_run(z, *pending, n_run - 1, n_run)
        return z[None]

    return jax.shard_map(layer, mesh=mesh,
                         in_specs=(row_spec, P(), head_cols, head_cols, head_cols, P('tp', None, None),
                                   P(), P(None, 'tp'), P(None, 'tp'), P('tp', None)),
                         out_specs=row_spec, check_vma=False)
```

time: 2510 us -> 1440 us (0.57)
  matrix products: 1160 us -> 0 us
  Pallas kernels: 0 us -> 861 us
  other arithmetic: 396 us -> 28.1 us
  waiting for transfers between devices: 839 us -> 484 us
  local copies, waits for them, and re-layouts: 76.4 us -> 26 us
  starting transfers between devices: 1.03 us -> 32.2 us
    dot_general x37 -> x0, matrix products: 1100 us -> none  [the longest x16 353 us: one_tile(): jnp.einsum('qgrd,kgd->gqrk', q_tile, keys, preferred_element_type=jnp.flo...]
    pallas_call x0 -> x34, Pallas kernels: none -> 861 us  [the longest x4 250 us: hidden(): pl.pallas_call(ordered(functools.partial(hidden_kernel, n_in=len(bs)), le...]
    ppermute x0 -> x55, waiting for transfers between devices: none -> 484 us  [send(): return lax.ppermute(v, *axis_pairs)]
    unnamed x8 -> x0, waiting for transfers between devices: 452 us -> none
    all_gather x4 -> x0, waiting for transfers between devices: 387 us -> none  [the longest x1 199 us: local_layer(): lax.all_gather(rms_norm(resid_rows, g_mlp), 'tp', axis=0, tiled=True)]
    reduce_sum x18 -> x0, other arithmetic: 308 us -> none  [the longest x16 294 us: one_tile(): row_sum = jnp.sum(weights, axis=-1, keepdims=True)]
    unnamed x2 -> x0, matrix products: 58.9 us -> none
    ppermute x0 -> x55, starting transfers between devices: none -> 32.2 us  [send(): return lax.ppermute(v, *axis_pairs)]
  transfers between devices with their start and end apart: 6 -> 55, of which waited for: 5 -> 27; matrix products, arithmetic and copies ran while one was open for 5% -> 3% of each run, Pallas kernels for 0% -> 35%
where the time goes in v2:
time: 1440 us; the launch traced here: 1430 us
  Pallas kernels  861 us (60%)
  waiting for transfers between devices  484 us (34%)
  starting transfers between devices  32.2 us (2%)
  other arithmetic  28.1 us (2%)
  local copies, waits for them, and re-layouts  26 us (2%)
    ppermute x55, waiting for transfers between devices, send(): return lax.ppermute(v, *axis_pairs)  484 us
    pallas_call x4, Pallas kernels, hidden(): pl.pallas_call(ordered(functools.partial(hidden_kernel, n_in=len(bs)), le...  250 us
    pallas_call x4, Pallas kernels, flash(): pl.pallas_call(ordered(functools.partial(flash_kernel, q_src=q_src, kv_sr...  233 us
    pallas_call x8, Pallas kernels, down(): pl.pallas_call(ordered(down_kernel, 2, after), grid=(dim // td,), in_spec...  154 us
    pallas_call x6, Pallas kernels, qkv(): pl.pallas_call(ordered(functools.partial(qkv_kernel, n_in=n_in, nq=nq), n...  101 us
    pallas_call x4, Pallas kernels, out_proj(): pl.pallas_call(ordered(functools.partial(out_kernel, n_w=len(ws)), 6 + le...  86.6 us
    ppermute x55, starting transfers between devices, send(): return lax.ppermute(v, *axis_pairs)  32.2 us
  transfers between devices with their start and end apart: 55, of which 27 were waited for; matrix products, arithmetic and copies ran while one was open for 3% of the time, Pallas kernels for 35%

profile of v2, /device:TPU:0, one launch (start us, length us, event | category | flops | bytes accessed | tf_op | source)
XLA Modules:
  0.0 1432.1 jit_solution(15153399063154184092)
XLA Ops:
  19.0 9.5 bitcast_dynamic-update-slice_fusion
  31.0 7.5 fusion
  43.7 22.6 %qkv.6 = (bf16[4,256,1024]{2,1,0:T(8,128)(2,1)}, bf16[4,2,256,256]{3,2,1,0:T(8,128)(2,1)}) custom-call(bf16[256,4096]{1,0:T(8,128)(2,1)} %norm.4.refs_2_.refs_0_, bf16[256,4096]{1,0:T(8,128)(2,1)} %norm.5.refs_2_.refs_1_, bf16[256,4096]{1,0:T(8,128)(2,1)} %norm.6.refs_2_, bf16[256,4096]{1,0:T(8,128)(2,1)} %norm.7.refs_3_, ...), custom_call_target="tpu_custom_call" | custom-call | flops 12884901888 | bytes 24117248 | tf_op jit(solution)/shard_map/qkv/pallas_call | solution.py:113
  66.3 22.4 %qkv.7 = (bf16[4,256,1024]{2,1,0:T(8,128)(2,1)}, bf16[4,2,256,256]{3,2,1,0:T(8,128)(2,1)}) custom-call(bf16[256,4096]{1,0:T(8,128)(2,1)} %collective-permute-done.refs_0_, bf16[256,4096]{1,0:T(8,128)(2,1)} %collective-permute-done.1.refs_1_, bf16[256,4096]{1,0:T(8,128)(2,1)} %collective-permute-done.2.refs_2_, ...), custom_call_target="tpu_custom_call" | custom-call | flops 12884901888 | bytes 24117248 | tf_op jit(solution)/shard_map/qkv/pallas_call | solution.py:113
  93.2 14.1 qkv.8
  107.3 29.8 %collective-permute-done.6.refs_0_ = bf16[256,4096]{1,0:T(8,128)(2,1)} collective-permute-done((bf16[256,4096]{1,0:T(8,128)(2,1)}, bf16[256,4096]{1,0:T(8,128)(2,1)}, u32[]{:S(2)}, u32[]{:S(2)}) %collective-permute-start.6) | collective-permute-done | bytes 2097184 | tf_op jit(solution)/shard_map/ppermute | solution.py:431
  141.6 14.1 qkv.9
  155.7 29.6 %collective-permute-done.8.refs_0_ = bf16[256,4096]{1,0:T(8,128)(2,1)} collective-permute-done((bf16[256,4096]{1,0:T(8,128)(2,1)S(1)}, bf16[256,4096]{1,0:T(8,128)(2,1)}, u32[]{:S(2)}, u32[]{:S(2)}) %collective-permute-start.8) | collective-permute-done | bytes 2097184 | tf_op jit(solution)/shard_map/ppermute | solution.py:431
  189.7 14.1 qkv.10
  203.9 29.6 %collective-permute-done.10.refs_0_ = bf16[256,4096]{1,0:T(8,128)(2,1)S(1)} collective-permute-done((bf16[256,4096]{1,0:T(8,128)(2,1)}, bf16[256,4096]{1,0:T(8,128)(2,1)S(1)}, u32[]{:S(2)}, u32[]{:S(2)}) %collective-permute-start.10) | collective-permute-done | bytes 2097184 | tf_op jit(solution)/shard_map/ppermute | solution.py:431
  242.6 14.1 qkv.11
  261.2 20.9 %collective-permute-done.13.refs_11_ = bf16[4,2,256,256]{3,2,1,0:T(8,128)(2,1)} collective-permute-done((bf16[4,2,256,256]{3,2,1,0:T(8,128)(2,1)}, bf16[4,2,256,256]{3,2,1,0:T(8,128)(2,1)}, u32[]{:S(2)}, u32[]{:S(2)}) %collective-permute-start.13) | collective-permute-done | bytes 1048608 | tf_op jit(solution)/shard_map/ppermute | solution.py:431
  285.0 8.4 collective-permute-done.14.refs_12_
  293.4 11.2 collective-permute-done.15.refs_13_
  304.6 11.1 collective-permute-done.16.refs_14_
  315.7 10.8 collective-permute-done.17.refs_15_
  327.3 56.0 %flash.4 = (bf16[256,1024]{1,0:T(8,128)(2,1)}, bf16[256,1024]{1,0:T(8,128)(2,1)}, bf16[256,1024]{1,0:T(8,128)(2,1)}, bf16[256,1024]{1,0:T(8,128)(2,1)}) custom-call(s32[608]{0:T(1024)} %dynamic-slice_reduce_fusion.refs_0_, bf16[4,256,1024]{2,1,0:T(8,128)(2,1)} %get-tuple-element.60.refs_1_, bf16[4,256,1024]{2,1,0:T(8,128)(2,1)} %get-tuple-element.62.refs_2_, ...), custom_call_target="tpu_custom_call" | custom-call | flops 34359738368 | bytes 12582912 | tf_op jit(solution)/shard_map/flash/pallas_call | solution.py:223
  384.8 55.5 %flash.5 = (bf16[256,1024]{1,0:T(8,128)(2,1)}, bf16[256,1024]{1,0:T(8,128)(2,1)}, bf16[256,1024]{1,0:T(8,128)(2,1)}, bf16[256,1024]{1,0:T(8,128)(2,1)}) custom-call(s32[608]{0:T(1024)} %dynamic-slice_reduce_fusion.refs_0_, bf16[4,256,1024]{2,1,0:T(8,128)(2,1)} %get-tuple-element.60.refs_1_, bf16[4,256,1024]{2,1,0:T(8,128)(2,1)} %get-tuple-element.62.refs_2_, ...), custom_call_target="tpu_custom_call" | custom-call | flops 34359738368 | bytes 12582912 | tf_op jit(solution)/shard_map/flash/pallas_call | solution.py:223
  440.3 60.9 %flash.6 = (bf16[256,1024]{1,0:T(8,128)(2,1)}, bf16[256,1024]{1,0:T(8,128)(2,1)}, bf16[256,1024]{1,0:T(8,128)(2,1)}, bf16[256,1024]{1,0:T(8,128)(2,1)}) custom-call(s32[608]{0:T(1024)} %dynamic-slice_reduce_fusion.refs_0_, bf16[4,256,1024]{2,1,0:T(8,128)(2,1)} %get-tuple-element.60.refs_1_, bf16[4,256,1024]{2,1,0:T(8,128)(2,1)} %get-tuple-element.62.refs_2_, ...), custom_call_target="tpu_custom_call" | custom-call | flops 38654705664 | bytes 12582912 | tf_op jit(solution)/shard_map/flash/pallas_call | solution.py:223
  516.6 10.2 collective-permute-done.20.refs_3_
  527.6 21.6 %outp.4 = (bf16[256,4096]{1,0:T(8,128)(2,1)}, bf16[256,4096]{1,0:T(8,128)(2,1)}) custom-call(bf16[256,1024]{1,0:T(8,128)(2,1)} %get-tuple-element.73.refs_16_.refs_0_, bf16[256,1024]{1,0:T(8,128)(2,1)} %copy-done.9, bf16[256,1024]{1,0:T(8,128)(2,1)} %copy-done.10, bf16[256,1024]{1,0:T(8,128)(2,1)} %copy-done.13, bf16[1024,4096]{1,0:T(8,128)(2,1)} %bitcast.24, ...), custom_call_target="tpu_custom_call" | custom-call | flops 8589934592 | bytes 41943040 | tf_op jit(solution)/shard_map/outp/pallas_call | solution.py:282
  549.8 60.8 %flash.7 = (bf16[256,1024]{1,0:T(8,128)(2,1)}, bf16[256,1024]{1,0:T(8,128)(2,1)}, bf16[256,1024]{1,0:T(8,128)(2,1)}, bf16[256,1024]{1,0:T(8,128)(2,1)}) custom-call(s32[608]{0:T(1024)} %dynamic-slice_reduce_fusion.refs_0_, bf16[4,256,1024]{2,1,0:T(8,128)(2,1)} %get-tuple-element.60.refs_1_, bf16[4,256,1024]{2,1,0:T(8,128)(2,1)} %get-tuple-element.62.refs_2_, ...), custom_call_target="tpu_custom_call" | custom-call | flops 38654705664 | bytes 12582912 | tf_op jit(solution)/shard_map/flash/pallas_call | solution.py:223
  615.7 10.5 collective-permute-done.30.refs_2_
  626.2 10.2 collective-permute-done.31.refs_3_
  637.2 21.7 %outp.5 = (bf16[256,4096]{1,0:T(8,128)(2,1)}, bf16[256,4096]{1,0:T(8,128)(2,1)}) custom-call(bf16[256,1024]{1,0:T(8,128)(2,1)} %get-tuple-element.81.refs_16_.refs_0_, bf16[256,1024]{1,0:T(8,128)(2,1)} %copy-done.12, bf16[256,1024]{1,0:T(8,128)(2,1)} %copy-done.14, bf16[256,1024]{1,0:T(8,128)(2,1)} %copy-done.17, bf16[1024,4096]{1,0:T(8,128)(2,1)} %bitcast.25, ...), custom_call_target="tpu_custom_call" | custom-call | flops 8589934592 | bytes 41943040 | tf_op jit(solution)/shard_map/outp/pallas_call | solution.py:282
  659.0 62.5 %hidden.4.refs_0_ = bf16[1024,3072]{1,0:T(8,128)(2,1)} custom-call(bf16[256,4096]{1,0:T(8,128)(2,1)} %get-tuple-element.84.refs_16_.refs_0_, bf16[256,4096]{1,0:T(8,128)(2,1)} %copy-done.20, bf16[256,4096]{1,0:T(8,128)(2,1)} %collective-permute-done.27.refs_2_, bf16[256,4096]{1,0:T(8,128)(2,1)} %collective-permute-done.28.refs_3_, ...), custom_call_target="tpu_custom_call" | custom-call | flops 51539607552 | bytes 65011712 | tf_op jit(solution)/shard_map/hidden/pallas_call | solution.py:314
  721.5 19.2 %down.8.refs_2_ = bf16[512,4096]{1,0:T(8,128)(2,1)} custom-call(bf16[1024,3072]{1,0:T(8,128)(2,1)} %hidden.4.refs_0_, bf16[3072,4096]{1,0:T(8,128)(2,1)} %refs_1_.15), custom_call_target="tpu_custom_call" | custom-call | flops 12884901888 | bytes 32505856 | tf_op jit(solution)/shard_map/down/pallas_call | solution.py:334
  743.3 46.4 %collective-permute-done.37.refs_1_ = bf16[256,4096]{1,0:T(8,128)(2,1)} collective-permute-done((bf16[256,4096]{1,0:T(8,128)(2,1)S(1)}, bf16[256,4096]{1,0:T(8,128)(2,1)}, u32[]{:S(2)}, u32[]{:S(2)}) %collective-permute-start.37) | collective-permute-done | bytes 2097184 | tf_op jit(solution)/shard_map/ppermute | solution.py:431
  789.6 19.1 %down.9.refs_0_ = bf16[512,4096]{1,0:T(8,128)(2,1)} custom-call(bf16[1024,3072]{1,0:T(8,128)(2,1)} %hidden.4.refs_0_, bf16[3072,4096]{1,0:T(8,128)(2,1)} %refs_1_.15, bf16[512,4096]{1,0:T(8,128)(2,1)} %down.8.refs_2_), custom_call_target="tpu_custom_call" | custom-call | flops 12884901888 | bytes 32505856 | tf_op jit(solution)/shard_map/down/pallas_call | solution.py:334
  814.6 7.8 collective-permute-done.42.refs_3_
  823.3 21.6 %outp.6 = (bf16[256,4096]{1,0:T(8,128)(2,1)}, bf16[256,4096]{1,0:T(8,128)(2,1)}) custom-call(bf16[256,1024]{1,0:T(8,128)(2,1)} %get-tuple-element.82.refs_12_.refs_0_, bf16[256,1024]{1,0:T(8,128)(2,1)} %copy-done.7, bf16[256,1024]{1,0:T(8,128)(2,1)} %copy-done.8, bf16[256,1024]{1,0:T(8,128)(2,1)} %copy-done.16, bf16[1024,4096]{1,0:T(8,128)(2,1)} %bitcast.26, ...), custom_call_target="tpu_custom_call" | custom-call | flops 8589934592 | bytes 41943040 | tf_op jit(solution)/shard_map/outp/pallas_call | solution.py:282
  844.9 62.7 %hidden.5.refs_0_ = bf16[1024,3072]{1,0:T(8,128)(2,1)} custom-call(bf16[256,4096]{1,0:T(8,128)(2,1)} %get-tuple-element.91.refs_6_.refs_0_, bf16[256,4096]{1,0:T(8,128)(2,1)} %collective-permute-done.37.refs_1_, bf16[256,4096]{1,0:T(8,128)(2,1)} %collective-permute-done.38.refs_2_, bf16[256,4096]{1,0:T(8,128)(2,1)} %collective-permute-done.39.refs_3_, ...), custom_call_target="tpu_custom_call" | custom-call | flops 51539607552 | bytes 65011712 | tf_op jit(solution)/shard_map/hidden/pallas_call | solution.py:314
  907.6 19.2 %down.10.refs_2_ = bf16[512,4096]{1,0:T(8,128)(2,1)} custom-call(bf16[1024,3072]{1,0:T(8,128)(2,1)} %hidden.5.refs_0_, bf16[3072,4096]{1,0:T(8,128)(2,1)} %refs_1_.15), custom_call_target="tpu_custom_call" | custom-call | flops 12884901888 | bytes 32505856 | tf_op jit(solution)/shard_map/down/pallas_call | solution.py:334
  929.6 46.6 %collective-permute-done.45.refs_1_ = bf16[256,4096]{1,0:T(8,128)(2,1)} collective-permute-done((bf16[256,4096]{1,0:T(8,128)(2,1)}, bf16[256,4096]{1,0:T(8,128)(2,1)}, u32[]{:S(2)}, u32[]{:S(2)}) %collective-permute-start.45) | collective-permute-done | bytes 2097184 | tf_op jit(solution)/shard_map/ppermute | solution.py:431
  976.2 19.1 %down.11.refs_1_ = bf16[512,4096]{1,0:T(8,128)(2,1)} custom-call(bf16[1024,3072]{1,0:T(8,128)(2,1)} %hidden.5.refs_0_, bf16[3072,4096]{1,0:T(8,128)(2,1)} %refs_1_.15, bf16[512,4096]{1,0:T(8,128)(2,1)} %down.10.refs_2_), custom_call_target="tpu_custom_call" | custom-call | flops 12884901888 | bytes 32505856 | tf_op jit(solution)/shard_map/down/pallas_call | solution.py:334
  1001.5 30.8 %collective-permute-done.35.refs_2_ = bf16[256,1024]{1,0:T(8,128)(2,1)S(1)} collective-permute-done((bf16[256,1024]{1,0:T(8,128)(2,1)}, bf16[256,1024]{1,0:T(8,128)(2,1)S(1)}, u32[]{:S(2)}, u32[]{:S(2)}) %collective-permute-start.35) | collective-permute-done | bytes 524320 | tf_op jit(solution)/shard_map/ppermute | solution.py:431
  1032.3 9.3 collective-permute-done.36.refs_3_
  1042.4 21.7 %outp.7 = (bf16[256,4096]{1,0:T(8,128)(2,1)}, bf16[256,4096]{1,0:T(8,128)(2,1)}) custom-call(bf16[256,1024]{1,0:T(8,128)(2,1)} %get-tuple-element.86.refs_12_.refs_0_, bf16[256,1024]{1,0:T(8,128)(2,1)} %copy-done.6, bf16[256,1024]{1,0:T(8,128)(2,1)} %copy-done.11, bf16[256,1024]{1,0:T(8,128)(2,1)} %copy-done.15, bf16[1024,4096]{1,0:T(8,128)(2,1)} %bitcast.27, ...), custom_call_target="tpu_custom_call" | custom-call | flops 8589934592 | bytes 41943040 | tf_op jit(solution)/shard_map/outp/pallas_call | solution.py:282
  1069.7 62.8 %hidden.6.refs_0_ = bf16[1024,3072]{1,0:T(8,128)(2,1)} custom-call(bf16[256,4096]{1,0:T(8,128)(2,1)} %get-tuple-element.100.refs_6_.refs_0_, bf16[256,4096]{1,0:T(8,128)(2,1)} %collective-permute-done.45.refs_1_, bf16[256,4096]{1,0:T(8,128)(2,1)} %collective-permute-done.46.refs_2_, bf16[256,4096]{1,0:T(8,128)(2,1)} %collective-permute-done.47.refs_3_, ...), custom_call_target="tpu_custom_call" | custom-call | flops 51539607552 | bytes 65011712 | tf_op jit(solution)/shard_map/hidden/pallas_call | solution.py:314
  1132.5 19.2 %down.12.refs_2_ = bf16[512,4096]{1,0:T(8,128)(2,1)} custom-call(bf16[1024,3072]{1,0:T(8,128)(2,1)} %hidden.6.refs_0_, bf16[3072,4096]{1,0:T(8,128)(2,1)} %refs_1_.15), custom_call_target="tpu_custom_call" | custom-call | flops 12884901888 | bytes 32505856 | tf_op jit(solution)/shard_map/down/pallas_call | solution.py:334
  1154.5 46.8 %collective-permute-done.50.refs_1_ = bf16[256,4096]{1,0:T(8,128)(2,1)} collective-permute-done((bf16[256,4096]{1,0:T(8,128)(2,1)}, bf16[256,4096]{1,0:T(8,128)(2,1)}, u32[]{:S(2)}, u32[]{:S(2)}) %collective-permute-start.50) | collective-permute-done | bytes 2097184 | tf_op jit(solution)/shard_map/ppermute | solution.py:431
  1201.3 19.1 %down.13.refs_1_ = bf16[512,4096]{1,0:T(8,128)(2,1)} custom-call(bf16[1024,3072]{1,0:T(8,128)(2,1)} %hidden.6.refs_0_, bf16[3072,4096]{1,0:T(8,128)(2,1)} %refs_1_.15, bf16[512,4096]{1,0:T(8,128)(2,1)} %down.12.refs_2_), custom_call_target="tpu_custom_call" | custom-call | flops 12884901888 | bytes 32505856 | tf_op jit(solution)/shard_map/down/pallas_call | solution.py:334
  1224.8 20.5 %collective-permute-done.44.refs_3_ = bf16[256,4096]{1,0:T(8,128)(2,1)} collective-permute-done((bf16[256,4096]{1,0:T(8,128)(2,1)S(1)}, bf16[256,4096]{1,0:T(8,128)(2,1)}, u32[]{:S(2)}, u32[]{:S(2)}) %collective-permute-start.44) | collective-permute-done | bytes 2097184 | tf_op jit(solution)/shard_map/ppermute | solution.py:431
  1250.9 62.5 %hidden.7.refs_0_ = bf16[1024,3072]{1,0:T(8,128)(2,1)} custom-call(bf16[256,4096]{1,0:T(8,128)(2,1)} %get-tuple-element.101.refs_4_.refs_0_, bf16[256,4096]{1,0:T(8,128)(2,1)} %collective-permute-done.50.refs_1_, bf16[256,4096]{1,0:T(8,128)(2,1)} %collective-permute-done.51.refs_2_, bf16[256,4096]{1,0:T(8,128)(2,1)} %collective-permute-done.52.refs_3_, ...), custom_call_target="tpu_custom_call" | custom-call | flops 51539607552 | bytes 65011712 | tf_op jit(solution)/shard_map/hidden/pallas_call | solution.py:314
  1313.4 19.5 %down.14.refs_2_ = bf16[512,4096]{1,0:T(8,128)(2,1)} custom-call(bf16[1024,3072]{1,0:T(8,128)(2,1)} %hidden.7.refs_0_, bf16[3072,4096]{1,0:T(8,128)(2,1)} %refs_1_.15), custom_call_target="tpu_custom_call" | custom-call | flops 12884901888 | bytes 32505856 | tf_op jit(solution)/shard_map/down/pallas_call | solution.py:334
  1334.4 19.2 %down.15.refs_1_ = bf16[512,4096]{1,0:T(8,128)(2,1)} custom-call(bf16[1024,3072]{1,0:T(8,128)(2,1)} %hidden.7.refs_0_, bf16[3072,4096]{1,0:T(8,128)(2,1)} %refs_1_.15, bf16[512,4096]{1,0:T(8,128)(2,1)} %down.14.refs_2_), custom_call_target="tpu_custom_call" | custom-call | flops 12884901888 | bytes 32505856 | tf_op jit(solution)/shard_map/down/pallas_call | solution.py:334
  1358.5 23.1 %collective-permute-done.49.refs_3_ = bf16[256,4096]{1,0:T(8,128)(2,1)} collective-permute-done((bf16[256,4096]{1,0:T(8,128)(2,1)S(1)}, bf16[256,4096]{1,0:T(8,128)(2,1)}, u32[]{:S(2)}, u32[]{:S(2)}) %collective-permute-start.49) | collective-permute-done | bytes 2097184 | tf_op jit(solution)/shard_map/ppermute | solution.py:431
  1387.2 38.9 %collective-permute-done.54.refs_3_ = bf16[256,4096]{1,0:T(8,128)(2,1)} collective-permute-done((bf16[256,4096]{1,0:T(8,128)(2,1)}, bf16[256,4096]{1,0:T(8,128)(2,1)}, u32[]{:S(2)}, u32[]{:S(2)}) %collective-permute-start.54) | collective-permute-done | bytes 2097184 | tf_op jit(solution)/shard_map/ppermute | solution.py:431
  (172 shorter events, 136.6 us)
Async XLA Ops:
  4.7 61.6 %collective-permute-start = (bf16[256,4096]{1,0:T(8,128)(2,1)}, bf16[256,4096]{1,0:T(8,128)(2,1)}, u32[]{:S(2)}, u32[]{:S(2)}) collective-permute-start(bf16[256,4096]{1,0:T(8,128)(2,1)} %norm.4.refs_2_.refs_0_), channel_id=1, source_target_pairs={{0,1},{1,0},{2,3},{3,2},{4,5},{5,4},{6,7},{7,6}} | collective-permute-start | bytes 6291464 | tf_op jit(solution)/shard_map/ppermute | solution.py:431
  5.5 83.2 %collective-permute-start.4 = (bf16[256,4096]{1,0:T(8,128)(2,1)}, bf16[256,4096]{1,0:T(8,128)(2,1)}, u32[]{:S(2)}, u32[]{:S(2)}) collective-permute-start(bf16[256,4096]{1,0:T(8,128)(2,1)} %norm.4.refs_2_.refs_0_), channel_id=1, source_target_pairs={{0,2},{1,3},{2,0},{3,1},{4,6},{5,7},{6,4},{7,5}} | collective-permute-start | bytes 6291464 | tf_op jit(solution)/shard_map/ppermute | solution.py:431
  11.4 54.9 %collective-permute-start.1 = (bf16[256,4096]{1,0:T(8,128)(2,1)}, bf16[256,4096]{1,0:T(8,128)(2,1)}, u32[]{:S(2)}, u32[]{:S(2)}) collective-permute-start(bf16[256,4096]{1,0:T(8,128)(2,1)} %norm.5.refs_2_.refs_1_), channel_id=1, source_target_pairs={{0,1},{1,0},{2,3},{3,2},{4,5},{5,4},{6,7},{7,6}} | collective-permute-start | bytes 6291464 | tf_op jit(solution)/shard_map/ppermute | solution.py:431
  15.0 51.3 %collective-permute-start.2 = (bf16[256,4096]{1,0:T(8,128)(2,1)}, bf16[256,4096]{1,0:T(8,128)(2,1)}, u32[]{:S(2)}, u32[]{:S(2)}) collective-permute-start(bf16[256,4096]{1,0:T(8,128)(2,1)} %norm.6.refs_2_), channel_id=1, source_target_pairs={{0,1},{1,0},{2,3},{3,2},{4,5},{5,4},{6,7},{7,6}} | collective-permute-start | bytes 6291464 | tf_op jit(solution)/shard_map/ppermute | solution.py:431
  18.7 47.6 %collective-permute-start.3 = (bf16[256,4096]{1,0:T(8,128)(2,1)}, bf16[256,4096]{1,0:T(8,128)(2,1)}, u32[]{:S(2)}, u32[]{:S(2)}) collective-permute-start(bf16[256,4096]{1,0:T(8,128)(2,1)} %norm.7.refs_3_), channel_id=1, source_target_pairs={{0,1},{1,0},{2,3},{3,2},{4,5},{5,4},{6,7},{7,6}} | collective-permute-start | bytes 6291464 | tf_op jit(solution)/shard_map/ppermute | solution.py:431
  89.0 48.1 %collective-permute-start.6 = (bf16[256,4096]{1,0:T(8,128)(2,1)}, bf16[256,4096]{1,0:T(8,128)(2,1)}, u32[]{:S(2)}, u32[]{:S(2)}) collective-permute-start(bf16[256,4096]{1,0:T(8,128)(2,1)} %norm.5.refs_2_.refs_1_), channel_id=1, source_target_pairs={{0,2},{1,3},{2,0},{3,1},{4,6},{5,7},{6,4},{7,5}} | collective-permute-start | bytes 6291464 | tf_op jit(solution)/shard_map/ppermute | solution.py:431
  137.1 48.1 %collective-permute-start.8 = (bf16[256,4096]{1,0:T(8,128)(2,1)S(1)}, bf16[256,4096]{1,0:T(8,128)(2,1)}, u32[]{:S(2)}, u32[]{:S(2)}) collective-permute-start(bf16[256,4096]{1,0:T(8,128)(2,1)S(1)} %copy-done), channel_id=1, source_target_pairs={{0,2},{1,3},{2,0},{3,1},{4,6},{5,7},{6,4},{7,5}} | collective-permute-start | bytes 6291464 | tf_op jit(solution)/shard_map/ppermute | solution.py:431
  185.2 48.3 %collective-permute-start.10 = (bf16[256,4096]{1,0:T(8,128)(2,1)}, bf16[256,4096]{1,0:T(8,128)(2,1)S(1)}, u32[]{:S(2)}, u32[]{:S(2)}) collective-permute-start(bf16[256,4096]{1,0:T(8,128)(2,1)} %norm.7.refs_3_), channel_id=1, source_target_pairs={{0,2},{1,3},{2,0},{3,1},{4,6},{5,7},{6,4},{7,5}} | collective-permute-start | bytes 6291464 | tf_op jit(solution)/shard_map/ppermute | solution.py:431
  233.5 26.2 %collective-permute-start.12 = (bf16[4,2,256,256]{3,2,1,0:T(8,128)(2,1)S(1)}, bf16[4,2,256,256]{3,2,1,0:T(8,128)(2,1)}, u32[]{:S(2)}, u32[]{:S(2)}) collective-permute-start(bf16[4,2,256,256]{3,2,1,0:T(8,128)(2,1)S(1)} %copy-done.22), channel_id=1, source_target_pairs={{0,4},{4,0},{1,5},{5,1},{2,6},{6,2},{3,7},{7,3}} | collective-permute-start | bytes 3145736 | tf_op jit(solution)/shard_map/ppermute | solution.py:431
  235.0 47.1 %collective-permute-start.13 = (bf16[4,2,256,256]{3,2,1,0:T(8,128)(2,1)}, bf16[4,2,256,256]{3,2,1,0:T(8,128)(2,1)}, u32[]{:S(2)}, u32[]{:S(2)}) collective-permute-start(bf16[4,2,256,256]{3,2,1,0:T(8,128)(2,1)} %get-tuple-element.63.refs_5_), channel_id=1, source_target_pairs={{0,4},{4,0},{1,5},{5,1},{2,6},{6,2},{3,7},{7,3}} | collective-permute-start | bytes 3145736 | tf_op jit(solution)/shard_map/ppermute | solution.py:431
  235.6 57.8 %collective-permute-start.14 = (bf16[2,2,256,256]{3,2,1,0:T(8,128)(2,1)}, bf16[2,2,256,256]{3,2,1,0:T(8,128)(2,1)}, u32[]{:S(2)}, u32[]{:S(2)}) collective-permute-start(bf16[2,2,256,256]{3,2,1,0:T(8,128)(2,1)} %get-tuple-element.66.refs_5_.refs_6_), channel_id=1, source_target_pairs={{0,4},{4,0},{1,5},{5,1},{2,6},{6,2},{3,7},{7,3}} | collective-permute-start | bytes 1572872 | tf_op jit(solution)/shard_map/ppermute | solution.py:431
  237.1 67.5 %collective-permute-start.15 = (bf16[2,2,256,256]{3,2,1,0:T(8,128)(2,1)}, bf16[2,2,256,256]{3,2,1,0:T(8,128)(2,1)}, u32[]{:S(2)}, u32[]{:S(2)}) collective-permute-start(bf16[2,2,256,256]{3,2,1,0:T(8,128)(2,1)} %get-tuple-element.68.refs_5_.refs_7_), channel_id=1, source_target_pairs={{0,4},{4,0},{1,5},{5,1},{2,6},{6,2},{3,7},{7,3}} | collective-permute-start | bytes 1572872 | tf_op jit(solution)/shard_map/ppermute | solution.py:431
  242.3 141.0 %collective-permute-start.22 = (bf16[512,4096]{1,0:T(8,128)(2,1)}, bf16[512,4096]{1,0:T(8,128)(2,1)}, u32[]{:S(2)}, u32[]{:S(2)}) collective-permute-start(bf16[512,4096]{1,0:T(8,128)(2,1)} %constant_dynamic-slice_fusion), channel_id=1, source_target_pairs={{0,2},{1,3},{2,0},{3,1},{4,6},{5,7},{6,4},{7,5}} | collective-permute-start | bytes 12582920 | tf_op jit(solution)/shard_map/ppermute | solution.py:431
  259.7 56.1 %collective-permute-start.16 = (bf16[2,2,256,256]{3,2,1,0:T(8,128)(2,1)S(1)}, bf16[2,2,256,256]{3,2,1,0:T(8,128)(2,1)S(1)}, u32[]{:S(2)}, u32[]{:S(2)}) collective-permute-start(bf16[2,2,256,256]{3,2,1,0:T(8,128)(2,1)S(1)} %copy-done.23), channel_id=1, source_target_pairs={{0,4},{4,0},{1,5},{5,1},{2,6},{6,2},{3,7},{7,3}} | collective-permute-start | bytes 1572872 | tf_op jit(solution)/shard_map/ppermute | solution.py:431
  282.1 44.4 %collective-permute-start.17 = (bf16[2,2,256,256]{3,2,1,0:T(8,128)(2,1)}, bf16[2,2,256,256]{3,2,1,0:T(8,128)(2,1)S(1)}, u32[]{:S(2)}, u32[]{:S(2)}) collective-permute-start(bf16[2,2,256,256]{3,2,1,0:T(8,128)(2,1)} %get-tuple-element.72.refs_9_.refs_16_), channel_id=1, source_target_pairs={{0,4},{4,0},{1,5},{5,1},{2,6},{6,2},{3,7},{7,3}} | collective-permute-start | bytes 1572872 | tf_op jit(solution)/shard_map/ppermute | solution.py:431
  293.4 233.5 %collective-permute-start.21 = (bf16[1024,4096]{1,0:T(8,128)(2,1)}, bf16[1024,4096]{1,0:T(8,128)(2,1)}, u32[]{:S(2)}, u32[]{:S(2)}) collective-permute-start(bf16[1024,4096]{1,0:T(8,128)(2,1)} %bitcast.23), channel_id=1, source_target_pairs={{0,1},{1,0},{2,3},{3,2},{4,5},{5,4},{6,7},{7,6}} | collective-permute-start | bytes 25165832 | tf_op jit(solution)/shard_map/ppermute | solution.py:431
  383.3 117.9 %collective-permute-start.23 = (bf16[512,4096]{1,0:T(8,128)(2,1)}, bf16[512,4096]{1,0:T(8,128)(2,1)}, u32[]{:S(2)}, u32[]{:S(2)}) collective-permute-start(bf16[512,4096]{1,0:T(8,128)(2,1)} %collective-permute-done.22.refs_6_), channel_id=1, source_target_pairs={{0,4},{4,0},{1,5},{5,1},{2,6},{6,2},{3,7},{7,3}} | collective-permute-start | bytes 12582920 | tf_op jit(solution)/shard_map/ppermute | solution.py:431
  384.8 142.0 %collective-permute-start.24 = (bf16[512,4096]{1,0:T(8,128)(2,1)}, bf16[512,4096]{1,0:T(8,128)(2,1)}, u32[]{:S(2)}, u32[]{:S(2)}) collective-permute-start(bf16[512,4096]{1,0:T(8,128)(2,1)} %collective-permute-done.22.refs_6_), channel_id=1, source_target_pairs={{0,1},{1,0},{2,3},{3,2},{4,5},{5,4},{6,7},{7,6}} | collective-permute-start | bytes 12582920 | tf_op jit(solution)/shard_map/ppermute | solution.py:431
  501.2 25.6 %collective-permute-start.25 = (bf16[512,4096]{1,0:T(8,128)(2,1)}, bf16[512,4096]{1,0:T(8,128)(2,1)}, u32[]{:S(2)}, u32[]{:S(2)}) collective-permute-start(bf16[512,4096]{1,0:T(8,128)(2,1)} %collective-permute-done.23.refs_7_), channel_id=1, source_target_pairs={{0,1},{1,0},{2,3},{3,2},{4,5},{5,4},{6,7},{7,6}} | collective-permute-start | bytes 12582920 | tf_op jit(solution)/shard_map/ppermute | solution.py:431
  501.8 14.8 %collective-permute-start.19 = (bf16[256,1024]{1,0:T(8,128)(2,1)S(1)}, bf16[256,1024]{1,0:T(8,128)(2,1)S(1)}, u32[]{:S(2)}, u32[]{:S(2)}) collective-permute-start(bf16[256,1024]{1,0:T(8,128)(2,1)S(1)} %copy-done.28), channel_id=1, source_target_pairs={{0,2},{1,3},{2,0},{3,1},{4,6},{5,7},{6,4},{7,5}} | collective-permute-start | bytes 1572872 | tf_op jit(solution)/shard_map/ppermute | solution.py:431
  509.5 17.3 %collective-permute-start.20 = (bf16[256,1024]{1,0:T(8,128)(2,1)S(1)}, bf16[256,1024]{1,0:T(8,128)(2,1)S(1)}, u32[]{:S(2)}, u32[]{:S(2)}) collective-permute-start(bf16[256,1024]{1,0:T(8,128)(2,1)S(1)} %copy-done.27), channel_id=1, source_target_pairs={{0,3},{1,2},{2,1},{3,0},{4,7},{5,6},{6,5},{7,4}} | collective-permute-start | bytes 1572872 | tf_op jit(solution)/shard_map/ppermute | solution.py:431
  549.2 61.4 %collective-permute-start.26 = (bf16[256,4096]{1,0:T(8,128)(2,1)}, bf16[256,4096]{1,0:T(8,128)(2,1)S(1)}, u32[]{:S(2)}, u32[]{:S(2)}) collective-permute-start(bf16[256,4096]{1,0:T(8,128)(2,1)} %get-tuple-element.84.refs_16_.refs_0_), channel_id=1, source_target_pairs={{0,2},{1,3},{2,0},{3,1},{4,6},{5,7},{6,4},{7,5}} | collective-permute-start | bytes 6291464 | tf_op jit(solution)/shard_map/ppermute | solution.py:431
  549.8 109.2 %collective-permute-start.27 = (bf16[256,4096]{1,0:T(8,128)(2,1)}, bf16[256,4096]{1,0:T(8,128)(2,1)}, u32[]{:S(2)}, u32[]{:S(2)}) collective-permute-start(bf16[256,4096]{1,0:T(8,128)(2,1)} %get-tuple-element.84.refs_16_.refs_0_), channel_id=1, source_target_pairs={{0,1},{1,0},{2,3},{3,2},{4,5},{5,4},{6,7},{7,6}} | collective-permute-start | bytes 6291464 | tf_op jit(solution)/shard_map/ppermute | solution.py:431
  610.6 48.4 %collective-permute-start.28 = (bf16[256,4096]{1,0:T(8,128)(2,1)S(1)}, bf16[256,4096]{1,0:T(8,128)(2,1)}, u32[]{:S(2)}, u32[]{:S(2)}) collective-permute-start(bf16[256,4096]{1,0:T(8,128)(2,1)S(1)} %collective-permute-done.26.refs_1_), channel_id=1, source_target_pairs={{0,1},{1,0},{2,3},{3,2},{4,5},{5,4},{6,7},{7,6}} | collective-permute-start | bytes 6291464 | tf_op jit(solution)/shard_map/ppermute | solution.py:431
  611.2 15.0 %collective-permute-start.30 = (bf16[256,1024]{1,0:T(8,128)(2,1)}, bf16[256,1024]{1,0:T(8,128)(2,1)S(1)}, u32[]{:S(2)}, u32[]{:S(2)}) collective-permute-start(bf16[256,1024]{1,0:T(8,128)(2,1)} %get-tuple-element.89), channel_id=1, source_target_pairs={{0,2},{1,3},{2,0},{3,1},{4,6},{5,7},{6,4},{7,5}} | collective-permute-start | bytes 1572872 | tf_op jit(solution)/shard_map/ppermute | solution.py:431
  612.6 23.8 %collective-permute-start.31 = (bf16[256,1024]{1,0:T(8,128)(2,1)}, bf16[256,1024]{1,0:T(8,128)(2,1)S(1)}, u32[]{:S(2)}, u32[]{:S(2)}) collective-permute-start(bf16[256,1024]{1,0:T(8,128)(2,1)} %get-tuple-element.90), channel_id=1, source_target_pairs={{0,3},{1,2},{2,1},{3,0},{4,7},{5,6},{6,5},{7,4}} | collective-permute-start | bytes 1572872 | tf_op jit(solution)/shard_map/ppermute | solution.py:431
  740.7 68.0 %collective-permute-start.32 = (bf16[512,4096]{1,0:T(8,128)(2,1)}, bf16[512,4096]{1,0:T(8,128)(2,1)}, u32[]{:S(2)}, u32[]{:S(2)}) collective-permute-start(bf16[512,4096]{1,0:T(8,128)(2,1)} %down.8.refs_2_), channel_id=1, source_target_pairs={{0,1},{1,0},{2,3},{3,2},{4,5},{5,4},{6,7},{7,6}} | collective-permute-start | bytes 12582920 | tf_op jit(solution)/shard_map/ppermute | solution.py:431
  741.0 48.6 %collective-permute-start.37 = (bf16[256,4096]{1,0:T(8,128)(2,1)S(1)}, bf16[256,4096]{1,0:T(8,128)(2,1)}, u32[]{:S(2)}, u32[]{:S(2)}) collective-permute-start(bf16[256,4096]{1,0:T(8,128)(2,1)S(1)} %copy-done.19), channel_id=1, source_target_pairs={{0,2},{1,3},{2,0},{3,1},{4,6},{5,7},{6,4},{7,5}} | collective-permute-start | bytes 6291464 | tf_op jit(solution)/shard_map/ppermute | solution.py:431
  742.5 72.1 %collective-permute-start.40 = (bf16[256,1024]{1,0:T(8,128)(2,1)}, bf16[256,1024]{1,0:T(8,128)(2,1)S(1)}, u32[]{:S(2)}, u32[]{:S(2)}) collective-permute-start(bf16[256,1024]{1,0:T(8,128)(2,1)} %get-tuple-element.97), channel_id=1, source_target_pairs={{0,1},{1,0},{2,3},{3,2},{4,5},{5,4},{6,7},{7,6}} | collective-permute-start | bytes 1572872 | tf_op jit(solution)/shard_map/ppermute | solution.py:431
  742.5 72.1 %collective-permute-start.41 = (bf16[256,1024]{1,0:T(8,128)(2,1)}, bf16[256,1024]{1,0:T(8,128)(2,1)S(1)}, u32[]{:S(2)}, u32[]{:S(2)}) collective-permute-start(bf16[256,1024]{1,0:T(8,128)(2,1)} %get-tuple-element.98), channel_id=1, source_target_pairs={{0,2},{1,3},{2,0},{3,1},{4,6},{5,7},{6,4},{7,5}} | collective-permute-start | bytes 1572872 | tf_op jit(solution)/shard_map/ppermute | solution.py:431
  743.1 101.8 %collective-permute-start.38 = (bf16[256,4096]{1,0:T(8,128)(2,1)S(1)}, bf16[256,4096]{1,0:T(8,128)(2,1)}, u32[]{:S(2)}, u32[]{:S(2)}) collective-permute-start(bf16[256,4096]{1,0:T(8,128)(2,1)S(1)} %copy-done.19), channel_id=1, source_target_pairs={{0,1},{1,0},{2,3},{3,2},{4,5},{5,4},{6,7},{7,6}} | collective-permute-start | bytes 6291464 | tf_op jit(solution)/shard_map/ppermute | solution.py:431
  789.6 55.3 %collective-permute-start.39 = (bf16[256,4096]{1,0:T(8,128)(2,1)}, bf16[256,4096]{1,0:T(8,128)(2,1)}, u32[]{:S(2)}, u32[]{:S(2)}) collective-permute-start(bf16[256,4096]{1,0:T(8,128)(2,1)} %collective-permute-done.37.refs_1_), channel_id=1, source_target_pairs={{0,1},{1,0},{2,3},{3,2},{4,5},{5,4},{6,7},{7,6}} | collective-permute-start | bytes 6291464 | tf_op jit(solution)/shard_map/ppermute | solution.py:431
  926.9 69.9 %collective-permute-start.43 = (bf16[512,4096]{1,0:T(8,128)(2,1)}, bf16[512,4096]{1,0:T(8,128)(2,1)}, u32[]{:S(2)}, u32[]{:S(2)}) collective-permute-start(bf16[512,4096]{1,0:T(8,128)(2,1)} %down.10.refs_2_), channel_id=1, source_target_pairs={{0,1},{1,0},{2,3},{3,2},{4,5},{5,4},{6,7},{7,6}} | collective-permute-start | bytes 12582920 | tf_op jit(solution)/shard_map/ppermute | solution.py:431
  927.4 48.8 %collective-permute-start.45 = (bf16[256,4096]{1,0:T(8,128)(2,1)}, bf16[256,4096]{1,0:T(8,128)(2,1)}, u32[]{:S(2)}, u32[]{:S(2)}) collective-permute-start(bf16[256,4096]{1,0:T(8,128)(2,1)} %get-tuple-element.100.refs_6_.refs_0_), channel_id=1, source_target_pairs={{0,2},{1,3},{2,0},{3,1},{4,6},{5,7},{6,4},{7,5}} | collective-permute-start | bytes 6291464 | tf_op jit(solution)/shard_map/ppermute | solution.py:431
  928.8 66.4 %collective-permute-start.34 = (bf16[256,1024]{1,0:T(8,128)(2,1)S(1)}, bf16[256,1024]{1,0:T(8,128)(2,1)S(1)}, u32[]{:S(2)}, u32[]{:S(2)}) collective-permute-start(bf16[256,1024]{1,0:T(8,128)(2,1)S(1)} %copy-done.24), channel_id=1, source_target_pairs={{0,1},{1,0},{2,3},{3,2},{4,5},{5,4},{6,7},{7,6}} | collective-permute-start | bytes 1572872 | tf_op jit(solution)/shard_map/ppermute | solution.py:431
  928.8 135.3 %collective-permute-start.33 = (bf16[256,4096]{1,0:T(8,128)(2,1)S(1)}, bf16[256,4096]{1,0:T(8,128)(2,1)}, u32[]{:S(2)}, u32[]{:S(2)}) collective-permute-start(bf16[256,4096]{1,0:T(8,128)(2,1)S(1)} %copy-done.1), channel_id=1, source_target_pairs={{0,2},{1,3},{2,0},{3,1},{4,6},{5,7},{6,4},{7,5}} | collective-permute-start | bytes 6291464 | tf_op jit(solution)/shard_map/ppermute | solution.py:431
  929.4 140.3 %collective-permute-start.46 = (bf16[256,4096]{1,0:T(8,128)(2,1)}, bf16[256,4096]{1,0:T(8,128)(2,1)}, u32[]{:S(2)}, u32[]{:S(2)}) collective-permute-start(bf16[256,4096]{1,0:T(8,128)(2,1)} %get-tuple-element.100.refs_6_.refs_0_), channel_id=1, source_target_pairs={{0,1},{1,0},{2,3},{3,2},{4,5},{5,4},{6,7},{7,6}} | collective-permute-start | bytes 6291464 | tf_op jit(solution)/shard_map/ppermute | solution.py:431
  976.2 93.5 %collective-permute-start.47 = (bf16[256,4096]{1,0:T(8,128)(2,1)}, bf16[256,4096]{1,0:T(8,128)(2,1)}, u32[]{:S(2)}, u32[]{:S(2)}) collective-permute-start(bf16[256,4096]{1,0:T(8,128)(2,1)} %collective-permute-done.45.refs_1_), channel_id=1, source_target_pairs={{0,1},{1,0},{2,3},{3,2},{4,5},{5,4},{6,7},{7,6}} | collective-permute-start | bytes 6291464 | tf_op jit(solution)/shard_map/ppermute | solution.py:431
  995.3 37.0 %collective-permute-start.35 = (bf16[256,1024]{1,0:T(8,128)(2,1)}, bf16[256,1024]{1,0:T(8,128)(2,1)S(1)}, u32[]{:S(2)}, u32[]{:S(2)}) collective-permute-start(bf16[256,1024]{1,0:T(8,128)(2,1)} %get-tuple-element.94), channel_id=1, source_target_pairs={{0,2},{1,3},{2,0},{3,1},{4,6},{5,7},{6,4},{7,5}} | collective-permute-start | bytes 1572872 | tf_op jit(solution)/shard_map/ppermute | solution.py:431
  996.7 44.9 %collective-permute-start.36 = (bf16[256,1024]{1,0:T(8,128)(2,1)}, bf16[256,1024]{1,0:T(8,128)(2,1)S(1)}, u32[]{:S(2)}, u32[]{:S(2)}) collective-permute-start(bf16[256,1024]{1,0:T(8,128)(2,1)} %get-tuple-element.95), channel_id=1, source_target_pairs={{0,3},{1,2},{2,1},{3,0},{4,7},{5,6},{6,5},{7,4}} | collective-permute-start | bytes 1572872 | tf_op jit(solution)/shard_map/ppermute | solution.py:431
  1151.8 68.6 %collective-permute-start.48 = (bf16[512,4096]{1,0:T(8,128)(2,1)}, bf16[512,4096]{1,0:T(8,128)(2,1)}, u32[]{:S(2)}, u32[]{:S(2)}) collective-permute-start(bf16[512,4096]{1,0:T(8,128)(2,1)} %down.12.refs_2_), channel_id=1, source_target_pairs={{0,1},{1,0},{2,3},{3,2},{4,5},{5,4},{6,7},{7,6}} | collective-permute-start | bytes 12582920 | tf_op jit(solution)/shard_map/ppermute | solution.py:431
  1152.5 48.8 %collective-permute-start.50 = (bf16[256,4096]{1,0:T(8,128)(2,1)}, bf16[256,4096]{1,0:T(8,128)(2,1)}, u32[]{:S(2)}, u32[]{:S(2)}) collective-permute-start(bf16[256,4096]{1,0:T(8,128)(2,1)} %get-tuple-element.101.refs_4_.refs_0_), channel_id=1, source_target_pairs={{0,2},{1,3},{2,0},{3,1},{4,6},{5,7},{6,4},{7,5}} | collective-permute-start | bytes 6291464 | tf_op jit(solution)/shard_map/ppermute | solution.py:431
  1154.0 91.3 %collective-permute-start.44 = (bf16[256,4096]{1,0:T(8,128)(2,1)S(1)}, bf16[256,4096]{1,0:T(8,128)(2,1)}, u32[]{:S(2)}, u32[]{:S(2)}) collective-permute-start(bf16[256,4096]{1,0:T(8,128)(2,1)S(1)} %copy-done.2), channel_id=1, source_target_pairs={{0,2},{1,3},{2,0},{3,1},{4,6},{5,7},{6,4},{7,5}} | collective-permute-start | bytes 6291464 | tf_op jit(solution)/shard_map/ppermute | solution.py:431
  1154.5 96.3 %collective-permute-start.51 = (bf16[256,4096]{1,0:T(8,128)(2,1)}, bf16[256,4096]{1,0:T(8,128)(2,1)}, u32[]{:S(2)}, u32[]{:S(2)}) collective-permute-start(bf16[256,4096]{1,0:T(8,128)(2,1)} %get-tuple-element.101.refs_4_.refs_0_), channel_id=1, source_target_pairs={{0,1},{1,0},{2,3},{3,2},{4,5},{5,4},{6,7},{7,6}} | collective-permute-start | bytes 6291464 | tf_op jit(solution)/shard_map/ppermute | solution.py:431
  1201.3 49.5 %collective-permute-start.52 = (bf16[256,4096]{1,0:T(8,128)(2,1)}, bf16[256,4096]{1,0:T(8,128)(2,1)}, u32[]{:S(2)}, u32[]{:S(2)}) collective-permute-start(bf16[256,4096]{1,0:T(8,128)(2,1)} %collective-permute-done.50.refs_1_), channel_id=1, source_target_pairs={{0,1},{1,0},{2,3},{3,2},{4,5},{5,4},{6,7},{7,6}} | collective-permute-start | bytes 6291464 | tf_op jit(solution)/shard_map/ppermute | solution.py:431
  1333.0 20.6 %collective-permute-start.53 = (bf16[512,4096]{1,0:T(8,128)(2,1)}, bf16[512,4096]{1,0:T(8,128)(2,1)}, u32[]{:S(2)}, u32[]{:S(2)}) collective-permute-start(bf16[512,4096]{1,0:T(8,128)(2,1)} %down.14.refs_2_), channel_id=1, source_target_pairs={{0,1},{1,0},{2,3},{3,2},{4,5},{5,4},{6,7},{7,6}} | collective-permute-start | bytes 12582920 | tf_op jit(solution)/shard_map/ppermute | solution.py:431
  1333.0 48.6 %collective-permute-start.49 = (bf16[256,4096]{1,0:T(8,128)(2,1)S(1)}, bf16[256,4096]{1,0:T(8,128)(2,1)}, u32[]{:S(2)}, u32[]{:S(2)}) collective-permute-start(bf16[256,4096]{1,0:T(8,128)(2,1)S(1)} %copy-done.3), channel_id=1, source_target_pairs={{0,2},{1,3},{2,0},{3,1},{4,6},{5,7},{6,4},{7,5}} | collective-permute-start | bytes 6291464 | tf_op jit(solution)/shard_map/ppermute | solution.py:431
  1357.9 68.1 %collective-permute-start.54 = (bf16[256,4096]{1,0:T(8,128)(2,1)}, bf16[256,4096]{1,0:T(8,128)(2,1)}, u32[]{:S(2)}, u32[]{:S(2)}) collective-permute-start(bf16[256,4096]{1,0:T(8,128)(2,1)} %add_convert_fusion.refs_5_), channel_id=1, source_target_pairs={{0,2},{1,3},{2,0},{3,1},{4,6},{5,7},{6,4},{7,5}} | collective-permute-start | bytes 6291464 | tf_op jit(solution)/shard_map/ppermute | solution.py:431
  (37 other events, 702.6 us)

commit v3 on v2

v3 whole, which is shorter than its diff:
```python
import functools
import math
import jax
import jax.numpy as jnp
import numpy as np
from jax import lax
from jax.experimental import pallas as pl
from jax.experimental.pallas import tpu as pltpu
from jax.sharding import PartitionSpec as P

NORM_EPS = 1e-5
ROPE_THETA = 500000.0
HD = 128
RUN = 256
NEG = -1e30
FAR = 1 << 29
LOG2E = math.log2(math.e)
DN = (((1,), (0,)), ((), ()))
VMEM = 67043328
BF = jnp.bfloat16
F32 = jnp.float32
ANY = pl.BlockSpec(memory_space=pltpu.HBM)


def params(n):
    return pltpu.CompilerParams(dimension_semantics=("arbitrary",) * n, vmem_limit_bytes=VMEM)


def rope_tables(positions):
    half = HD // 2
    inv_freq = ROPE_THETA ** (-2.0 * jnp.arange(half, dtype=F32) / HD)
    angles = inv_freq[:, None] * positions.astype(F32)[..., None, :]
    return jnp.cos(angles), jnp.sin(angles)


def norm_rows(rows, gain):
    f = rows.astype(F32)
    mean_sq = jnp.mean(f * f, axis=-1, keepdims=True)
    return (f * lax.rsqrt(mean_sq + NORM_EPS) * gain.astype(F32)).astype(BF)


def ordered(kernel, n_in, after):
    n = len(after)
    return lambda *refs: kernel(*refs[:n_in], *refs[n_in + n:])


def load_all(pairs, sem):
    copies = [pltpu.make_async_copy(src, dst, sem.at[i]) for i, (src, dst) in enumerate(pairs)]
    for cp in copies:
        cp.start()
    for cp in copies:
        cp.wait()


def norm_kernel(x_ref, g_ref, o_ref):
    o_ref[...] = norm_rows(x_ref[...], g_ref[...])


def norm_run(x_rows, gain, j, after=(), tile=128):
    dim = x_rows.shape[1]
    per = RUN // tile
    return pl.pallas_call(
        ordered(norm_kernel, 2, after), grid=(per,),
        in_specs=[pl.BlockSpec((tile, dim), lambda i: (j * per + i, 0)), pl.BlockSpec((1, dim), lambda i: (0, 0))]
        + [ANY] * len(after),
        out_specs=pl.BlockSpec((tile, dim), lambda i: (i, 0)),
        out_shape=jax.ShapeDtypeStruct((RUN, dim), BF),
        name="norm", compiler_params=params(1),
        cost_estimate=pl.CostEstimate(flops=8 * RUN * dim, transcendentals=0, bytes_accessed=4 * RUN * dim),
    )(x_rows, gain, *after)


def qkv_kernel(*refs, n_in, nq):
    a_refs = refs[:n_in]
    w_ref, cos_ref, sin_ref, q_ref, kv_ref, a_scr, sem = refs[n_in:]
    n = pl.program_id(0)

    @pl.when(n == 0)
    def _():
        load_all([(r, a_scr.at[pl.ds(i * RUN, RUN), :]) for i, r in enumerate(a_refs)], sem)

    r = jnp.dot(a_scr[...], w_ref[...], preferred_element_type=F32)

    def piece(i, h):
        return r[i * RUN:(i + 1) * RUN, h * HD:(h + 1) * HD].T

    def rope(i, h):
        f = piece(i, h).astype(BF).astype(F32)
        lo, hi, cos, sin = f[:HD // 2], f[HD // 2:], cos_ref[i], sin_ref[i]
        return jnp.concatenate([lo * cos - hi * sin, hi * cos + lo * sin], axis=0)

    parts = [(i, h) for i in range(n_in) for h in range(2)]

    @pl.when(n < nq)
    def _():
        for i, h in parts:
            q_ref[i, h * HD:(h + 1) * HD, :] = rope(i, h).astype(BF)

    @pl.when(n == nq)
    def _():
        for i, h in parts:
            kv_ref[i, 0, :, h * HD:(h + 1) * HD] = rope(i, h).T.astype(BF)

    @pl.when(n == nq + 1)
    def _():
        for i, h in parts:
            kv_ref[i, 0, h * HD:(h + 1) * HD, :] = piece(i, h).astype(BF)


def qkv(rows, w_all, cos, sin, first_run, after=()):
    n_in = len(rows)
    dim, cols = w_all.shape
    nq = cols // 256 - 2
    at = first_run // n_in
    tab = pl.BlockSpec((n_in, HD // 2, RUN), lambda n: (at, 0, 0))
    return pl.pallas_call(
        ordered(functools.partial(qkv_kernel, n_in=n_in, nq=nq), n_in + 3, after),
        grid=(nq + 2,),
        in_specs=[ANY] * n_in + [pl.BlockSpec((dim, 256), lambda n: (0, n)), tab, tab] + [ANY] * len(after),
        out_specs=[pl.BlockSpec((n_in, 256, RUN), lambda n: (0, jnp.minimum(n, nq - 1), 0)),
                   pl.BlockSpec((n_in, 1, 256, 256), lambda n: (0, jnp.maximum(n - nq, 0), 0, 0))],
        out_shape=[jax.ShapeDtypeStruct((n_in, nq * 256, RUN), BF), jax.ShapeDtypeStruct((n_in, 2, 256, 256), BF)],
        scratch_shapes=[pltpu.VMEM((n_in * RUN, dim), BF), pltpu.SemaphoreType.DMA((n_in,))],
        name="qkv", compiler_params=params(1),
        cost_estimate=pl.CostEstimate(flops=2 * n_in * RUN * dim * cols, transcendentals=0,
                                      bytes_accessed=2 * (n_in * RUN * dim + dim * cols + n_in * RUN * cols)),
    )(*rows, w_all, cos, sin, *after)


BLK = 12
MASK0, MASK1, LAST = 1, 2, 4


def flash_kernel(tab_ref, *refs, q_src, kv_src, n_q, n_kv, base, G, n_tiles, n_heads):
    qs, kvs, outs = refs[:n_q], refs[n_q:n_q + n_kv], refs[n_q + n_kv:n_q + n_kv + n_tiles]
    q_scr, kv_scr, o_scr, s_scr, mb_scr, acc_scr, m_scr, l_scr, q_sem, kv_sem, o_sem = refs[n_q + n_kv + n_tiles:]
    T = RUN
    c = (HD ** -0.5) * LOG2E
    n_blocks = tab_ref[base]
    row0 = base + 1 + n_tiles

    q_copies = [pltpu.make_async_copy(qs[a].at[i], q_scr.at[t], q_sem.at[t]) for t, (a, i) in enumerate(q_src)]
    kv_copies = [pltpu.make_async_copy(kvs[a].at[i], kv_scr.at[r], kv_sem.at[r]) for r, (a, i) in enumerate(kv_src)]
    for cp in q_copies + kv_copies:
        cp.start()
    for cp in q_copies:
        cp.wait()

    def clear():
        acc_scr[...] = jnp.zeros_like(acc_scr)
        l_scr[...] = jnp.zeros_like(l_scr)
        m_scr[...] = jnp.full_like(m_scr, NEG)

    def block(i):
        g = lax.div(i, n_blocks)
        return row0 + BLK * (i - g * n_blocks), g

    def arrived(have, need):
        def one(r, carry):
            pltpu.make_async_copy(kv_scr.at[r], kv_scr.at[r], kv_sem.at[r]).wait()
            return carry

        lax.fori_loop(have, need, one, 0)
        return jnp.maximum(have, need)

    def put(s, slot):
        s_scr[slot] = s
        mb = jnp.max(s.reshape(2 * RUN // 8, 8, T), axis=0)
        for r in (4, 2, 1):
            mb = jnp.maximum(mb, pltpu.roll(mb, r, 0))
        mb_scr[slot] = mb

    def stage_a(row, g, it, h):
        col = pl.multiple_of(g * HD, HD)
        qt = q_scr[tab_ref[row], pl.ds(pl.multiple_of((g * G + h) * HD, HD), HD), :]
        put(jnp.concatenate([lax.dot_general(kv_scr[tab_ref[row + 3 + 2 * it + k], 0, :, pl.ds(col, HD)], qt, DN,
                                             preferred_element_type=F32) for k in range(2)], axis=0), it * G + h)

    def stage_b(row, g, it, h):
        slot = it * G + h
        col = pl.multiple_of(g * HD, HD)
        m_prev = m_scr[h]
        m_new = jnp.maximum(m_prev, mb_scr[slot])
        m_scr[h] = m_new
        m_c = m_new * c
        p = jnp.exp2(s_scr[slot].reshape(2 * RUN // 8, 8, T) * c - m_c[None])
        alpha = jnp.exp2(m_prev * c - m_c)
        l_scr[h] = l_scr[h] * alpha + jnp.sum(p, axis=0)
        pb = p.reshape(2 * RUN, T).astype(BF)
        pv = sum(lax.dot_general(kv_scr[tab_ref[row + 3 + 2 * it + k], 1, pl.ds(col, HD), :], pb[k * RUN:(k + 1) * RUN], DN,
                                 preferred_element_type=F32) for k in range(2))
        acc_scr[h] = (acc_scr[h].reshape(HD // 8, 8, T) * alpha[None]).reshape(HD, T) + pv

    def mask_item(row, it):
        key = lax.broadcasted_iota(jnp.int32, (RUN, T), 0)
        qry = lax.broadcasted_iota(jnp.int32, (RUN, T), 1) + tab_ref[base + 1 + tab_ref[row]]
        mask = jnp.concatenate([key + tab_ref[row + 7 + 2 * it + k] <= qry for k in range(2)], axis=0)
        for h in range(G):
            put(jnp.where(mask, s_scr[it * G + h], NEG), it * G + h)

    row, g = block(0)
    have = arrived(0, tab_ref[row + 2])
    clear()
    for it in range(2):
        for h in range(G):
            stage_a(row, g, it, h)

    def body(i, have):
        row, g = block(i)
        nrow, ng = block(jnp.minimum(i + 1, n_heads * n_blocks - 1))
        have = arrived(have, tab_ref[nrow + 2])
        flags = tab_ref[row + 1]

        @pl.when((flags & MASK0) != 0)
        def _():
            mask_item(row, 0)

        @pl.when((flags & MASK1) != 0)
        def _():
            mask_item(row, 1)

        for it in range(2):
            for h in range(G):
                stage_b(row, g, it, h)
                stage_a(nrow, ng, it, h)

        @pl.when((flags & LAST) != 0)
        def _():
            tile = tab_ref[row]
            for h in range(G):
                l = jnp.sum(l_scr[h], axis=0, keepdims=True)
                o_scr[tile, :, pl.ds(pl.multiple_of((g * G + h) * HD, HD), HD)] = (acc_scr[h] / l).T.astype(BF)
            clear()
            for k in range(n_tiles):
                @pl.when((tile == k) & (g == n_heads - 1))
                def _():
                    pltpu.make_async_copy(o_scr.at[k], outs[k], o_sem.at[k]).start()

        return have

    have = lax.fori_loop(0, n_heads * n_blocks, body, have)
    arrived(have, len(kv_src))
    for k in range(n_tiles):
        pltpu.make_async_copy(o_scr.at[k], outs[k], o_sem.at[k]).wait()


def flash(tab, qs, q_src, kvs, *, base, work, after=()):
    nq = qs[0].shape[1]
    n_heads = 2
    G = nq // HD // n_heads
    n_tiles = len(q_src)
    kv_src = [(a, i) for a, kv in enumerate(kvs) for i in range(kv.shape[0])]
    n_runs = len(kv_src)
    slots = 2 * G
    return pl.pallas_call(
        ordered(functools.partial(flash_kernel, q_src=q_src, kv_src=kv_src, n_q=len(qs), n_kv=len(kvs), base=base, G=G,
                                  n_tiles=n_tiles, n_heads=n_heads), 1 + len(qs) + len(kvs), after),
        grid_spec=pltpu.PrefetchScalarGridSpec(
            num_scalar_prefetch=1, grid=(),
            in_specs=[ANY] * (len(qs) + len(kvs) + len(after)),
            out_specs=[ANY] * n_tiles,
            scratch_shapes=[pltpu.VMEM((n_tiles, nq, RUN), BF),
                            pltpu.VMEM((n_runs, 2, 256, 256), BF),
                            pltpu.VMEM((n_tiles, RUN, nq), BF),
                            pltpu.VMEM((slots, 2 * RUN, RUN), F32),
                            pltpu.VMEM((slots, 8, RUN), F32),
                            pltpu.VMEM((G, HD, RUN), F32),
                            pltpu.VMEM((G, 8, RUN), F32),
                            pltpu.VMEM((G, 8, RUN), F32),
                            pltpu.SemaphoreType.DMA((n_tiles,)),
                            pltpu.SemaphoreType.DMA((n_runs,)),
                            pltpu.SemaphoreType.DMA((n_tiles,))]),
        out_shape=[jax.ShapeDtypeStruct((RUN, nq), BF)] * n_tiles,
        name="flash", compiler_params=pltpu.CompilerParams(vmem_limit_bytes=VMEM),
        cost_estimate=pl.CostEstimate(flops=8 * work * RUN * RUN * nq, transcendentals=work * RUN * RUN * nq // HD,
                                      bytes_accessed=n_runs * 2 * 256 * 256 * 2 + 4 * n_tiles * RUN * nq),
    )(tab, *qs, *kvs, *after)


def out_kernel(*refs, n_w, n_run):
    o_refs, w_refs = refs[:4 * n_run], refs[4 * n_run:4 * n_run + n_w]
    x_ref, g_ref, y_ref = refs[4 * n_run + n_w:4 * n_run + n_w + 3]
    b_refs, (o_scr, sem) = refs[4 * n_run + n_w + 3:-2], refs[-2:]
    n = pl.program_id(0)
    tn = w_refs[0].shape[1]
    width = o_refs[0].shape[1]
    half = width // 2

    @pl.when(n == 0)
    def _():
        mine = lax.axis_index('cp')
        pairs = []
        for i in range(n_run):
            rows = pl.ds(i * RUN, RUN)
            os = o_refs[4 * i:4 * i + 4]
            pairs += [(os[0], o_scr.at[rows, pl.ds(0, width)]), (os[1], o_scr.at[rows, pl.ds(width, width)])]
            for k in range(2, 4):
                for p, part in enumerate((mine, 1 - mine)):
                    pairs.append((os[k].at[:, pl.ds(pl.multiple_of(part * half, half), half)],
                                  o_scr.at[rows, pl.ds(k * width + p * half, half)]))
        load_all(pairs, sem)

    acc, k0 = None, 0
    for w in w_refs:
        d = jnp.dot(o_scr[:, k0:k0 + w.shape[0]], w[...], preferred_element_type=F32)
        acc = d if acc is None else acc + d
        k0 += w.shape[0]
    cols = pl.ds(pl.multiple_of(n * tn, tn), tn)
    y_ref[:, cols] = (x_ref[:, cols].astype(F32) + acc.astype(BF).astype(F32)).astype(BF)

    @pl.when(n == pl.num_programs(0) - 1)
    def _():
        for k in range(n_run):
            def rows64(i, carry):
                at = pl.multiple_of(i * 64, 64)
                b_refs[k][pl.ds(at, 64), :] = norm_rows(y_ref[pl.ds(k * RUN + at, 64), :], g_ref[...])
                return carry

            lax.fori_loop(0, RUN // 64, rows64, 0)


def out_proj(os, ws, x_rows, gain, at, after=(), tn=256):
    dim = x_rows.shape[1]
    n_run = len(os) // 4
    width = os[0].shape[1]
    rows = n_run * RUN
    whole = lambda m, s: pl.BlockSpec((m, dim), lambda n: (s, 0))
    return pl.pallas_call(
        ordered(functools.partial(out_kernel, n_w=len(ws), n_run=n_run), len(os) + len(ws) + 2, after),
        grid=(dim // tn,),
        in_specs=[ANY] * len(os) + [pl.BlockSpec((w.shape[0], tn), lambda n: (0, n)) for w in ws]
        + [whole(rows, at), pl.BlockSpec((1, dim), lambda n: (0, 0))] + [ANY] * len(after),
        out_specs=[whole(rows, 0)] + [whole(RUN, 0)] * n_run,
        out_shape=[jax.ShapeDtypeStruct((rows, dim), BF)] + [jax.ShapeDtypeStruct((RUN, dim), BF)] * n_run,
        scratch_shapes=[pltpu.VMEM((rows, 4 * width), BF), pltpu.SemaphoreType.DMA((6 * n_run,))],
        name="outp", compiler_params=params(1),
        cost_estimate=pl.CostEstimate(flops=8 * rows * width * dim, transcendentals=0,
                                      bytes_accessed=8 * width * dim + 8 * rows * dim),
    )(*os, *ws, x_rows, gain, *after)


def mlp_kernel(*refs, n_in, tn, nk):
    b_refs = refs[:n_in]
    wg_ref, wu_ref, wd_ref, keep_ref, send_ref, b_scr, u_scr, sem = refs[n_in:]
    i = pl.program_id(0)

    def gated(rows, cols):
        b = b_scr[rows, :]
        gate = jnp.dot(b, wg_ref[...], preferred_element_type=F32)
        up = jnp.dot(b, wu_ref[...], preferred_element_type=F32)
        u_scr[rows, cols] = (jax.nn.silu(gate) * up).astype(BF)

    @pl.when(i == 0)
    def _():
        copies = [pltpu.make_async_copy(r, b_scr.at[pl.ds(k * RUN, RUN), :], sem.at[k]) for k, r in enumerate(b_refs)]
        for cp in copies:
            cp.start()

        def one(k, carry):
            rows = pl.ds(pl.multiple_of(k * RUN, RUN), RUN)
            pltpu.make_async_copy(b_scr.at[rows, :], b_scr.at[rows, :], sem.at[k]).wait()
            gated(rows, pl.ds(0, tn))
            return carry

        lax.fori_loop(0, n_in, one, 0)

    @pl.when((i > 0) & (i < nk))
    def _():
        gated(slice(None), pl.ds(pl.multiple_of(i * tn, tn), tn))

    @pl.when(i >= nk)
    def _():
        d = jnp.dot(u_scr[...], wd_ref[...], preferred_element_type=F32).astype(BF)
        half = d.shape[0] // 2
        keep_ref[...] = d[:half]
        send_ref[...] = d[half:]


def mlp(bs, wg, wu, wd, after=(), tn=256, td=256):
    rows, dim = RUN * len(bs), bs[0].shape[1]
    ffn = wg.shape[1]
    nk, nd = ffn // tn, dim // td
    up = lambda i: (0, jnp.minimum(i, nk - 1))
    dn = lambda i: (0, jnp.maximum(i - nk, 0))
    return pl.pallas_call(
        ordered(functools.partial(mlp_kernel, n_in=len(bs), tn=tn, nk=nk), len(bs) + 3, after),
        grid=(nk + nd,),
        in_specs=[ANY] * len(bs) + [pl.BlockSpec((dim, tn), up), pl.BlockSpec((dim, tn), up), pl.BlockSpec((ffn, td), dn)]
        + [ANY] * len(after),
        out_specs=[pl.BlockSpec((rows // 2, td), dn)] * 2,
        out_shape=[jax.ShapeDtypeStruct((rows // 2, dim), BF)] * 2,
        scratch_shapes=[pltpu.VMEM((rows, dim), BF), pltpu.VMEM((rows, ffn), BF), pltpu.SemaphoreType.DMA((len(bs),))],
        name="mlp", compiler_params=params(1),
        cost_estimate=pl.CostEstimate(flops=6 * rows * dim * ffn, transcendentals=rows * ffn,
                                      bytes_accessed=6 * dim * ffn + 4 * rows * dim),
    )(*bs, wg, wu, wd, *after)


def sum_kernel(*refs):
    p_ref, r_ref, t_ref, y_ref, z_ref = refs[-5:]
    total = p_ref[...].astype(F32) + r_ref[...].astype(F32) + t_ref[...].astype(F32)
    z_ref[...] = (y_ref[...].astype(F32) + total.astype(BF).astype(F32)).astype(BF)


def sum_run(z, keep, recv, far, y, y_at, j, n_runs, after=(), tile=64):
    dim = y.shape[1]
    per = RUN // tile
    spec = pl.BlockSpec((tile, dim), lambda i: (i, 0))
    prev = () if z is None else (z,)
    return pl.pallas_call(
        ordered(sum_kernel, len(prev) + 4, after), grid=(per,),
        in_specs=[ANY] * len(prev) + [spec] * 3 + [pl.BlockSpec((tile, dim), lambda i: (y_at * per + i, 0))] + [ANY] * len(after),
        out_specs=pl.BlockSpec((tile, dim), lambda i: (j * per + i, 0)),
        out_shape=jax.ShapeDtypeStruct((n_runs * RUN, dim), BF),
        input_output_aliases={0: 0} if prev else {},
        name="zsum", compiler_params=params(1),
        cost_estimate=pl.CostEstimate(flops=6 * RUN * dim, transcendentals=0, bytes_accessed=10 * RUN * dim),
    )(*prev, keep, recv, far, y, *after)


def run_positions(xi, ci, y, cps, piece):
    def start(x, c):
        return (y if x == 0 else 2 * cps - 1 - y) * piece + c * (piece // 2)

    per = piece // 2 // RUN
    out = [start(xi, ci) + RUN * j for j in range(per)] + [start(xi, 1 - ci) + RUN * j for j in range(per)]
    for j in range(per):
        out += [start(1 - xi, ci) + RUN * j, start(1 - xi, 1 - ci) + RUN * j]
    return out


def block_list(tile, ids, pos, diag):
    runs = [(r, pos[r]) for r in ids]
    if diag is not None:
        n_tail = (len(runs) % 4) + 1
        tail = [(diag, pos[diag])] + runs[len(runs) - (n_tail - 1):]
        runs = runs[:len(runs) - (n_tail - 1)]
    else:
        n_tail = len(runs) % 4
        tail = runs[len(runs) - n_tail:]
        runs = runs[:len(runs) - n_tail]
    blocks = [[0, runs[i:i + 4]] for i in range(0, len(runs), 4)]
    if tail:
        full = tail + [(tail[0][0], FAR)] * (4 - len(tail))
        flags = (MASK0 if diag is not None or len(tail) < 2 else 0) | (MASK1 if len(tail) < 4 else 0)
        blocks.append([flags, full])
    blocks[-1][0] |= LAST
    return [[tile, flags, 0] + [r for r, _ in four] + [p for _, p in four] + [0] for flags, four in blocks]


def call_table(tiles, pos, pairs):
    rows, most = [], 0
    for t, tile in enumerate(tiles):
        ids, own = pairs[t]
        rows += block_list(t, ids, pos, tile if own else None)
    for row in rows:
        most = max(most, max(row[3:7]) + 1)
        row[2] = most
    return [len(rows)] + [pos[t] for t in tiles] + [v for row in rows for v in row], len(rows)


def work_tables(cps, piece):
    per = piece // 2 // RUN
    calls = [[j, per + j, 2 * per + 2 * j, 2 * per + 2 * j + 1] for j in range(per)]
    tabs, all_runs, sizes = [], [], []
    for y in range(cps):
        for xi in range(2):
            for ci in range(2):
                mine = run_positions(xi, ci, y, cps, piece)
                pos = mine + run_positions(xi, ci, 1 - y, cps, piece)
                all_runs.append(mine)
                tabs.append([])
                sizes.append([])
                for tiles in calls:
                    pairs = [([r for r in range(len(pos)) if pos[r] < pos[t]], True) for t in tiles]
                    tab, n = call_table(tiles, pos, pairs)
                    tabs[-1].append(tab)
                    sizes[-1].append(n)
    widths = [max(len(t[k]) for t in tabs) for k in range(len(calls))]
    flat = [[v for k, t in enumerate(tab) for v in t + [0] * (widths[k] - len(t))] for tab in tabs]
    bases = [sum(widths[:k]) for k in range(len(calls))]
    return np.array(flat, np.int32), np.array(all_runs, np.int32), bases, np.array(sizes).max(0) * 4


def solution(mesh):
    cps = mesh.shape['cp']
    row_spec = P('dp', ('cp', 'tp'), None)
    head_cols = P(None, 'tp', None)
    n_tp = mesh.shape['tp']

    over_core, over_x, over_both = (('tp', [(t, t ^ k) for t in range(n_tp)]) for k in (1, 2, 3))
    over_y = ('cp', [(i, i ^ 1) for i in range(cps)])

    def layer(x, g_attn, w_q, w_k, w_v, w_o, g_mlp, w_gate, w_up, w_down):
        x_rows = x[0]
        dim = x_rows.shape[1]
        n_run = x_rows.shape[0] // RUN
        piece = 2 * x_rows.shape[0]
        t_id, y_id = lax.axis_index('tp'), lax.axis_index('cp')
        np_tab, np_runs, bases, work = work_tables(cps, piece)
        dev = y_id * n_tp + t_id
        tab = lax.dynamic_index_in_dim(jnp.asarray(np_tab), dev, 0, keepdims=False)
        run_pos = lax.dynamic_index_in_dim(jnp.asarray(np_runs), dev, 0, keepdims=False)

        def tied(v, *others):
            return lax.optimization_barrier((v, *others))[0]

        def send(axis_pairs, v):
            return lax.ppermute(v, *axis_pairs)

        ga, gm = g_attn.reshape(1, dim), g_mlp.reshape(1, dim)
        own = []
        for j in range(n_run):
            own.append(norm_run(x_rows, ga, j, after=own[-1:]))
        far = [send(over_x, own[j]) for j in range(n_run)]
        mate = [send(over_core, own[j]) for j in range(n_run)]

        w_all = jnp.concatenate([tied(w, own[-1]).reshape(dim, -1) for w in (w_q, w_k, w_v)], axis=1)
        cos, sin = rope_tables(tied(run_pos, own[-1])[:, None] + jnp.arange(RUN, dtype=jnp.int32)[None, :])

        q_own, kv_own = qkv(own, w_all, cos, sin, 0)
        q_mate, kv_mate = qkv(mate, w_all, cos, sin, n_run, after=(kv_own,))
        kvs = [kv_own, kv_mate]
        q_far = []
        for j in range(n_run):
            here = tied(far[j], kvs[-1])
            q, kv = qkv([here, send(over_core, here)], w_all, cos, sin, 2 * n_run + 2 * j,
                         after=(kvs[-1],))
            q_far.append(q)
            kvs.append(kv)
        gate, last = kvs[3], kvs[-1]
        kvs = kvs + [send(over_y, kv) for kv in kvs]

        wo = w_o.reshape(-1, dim)
        half = wo.shape[0] // 2
        wo_gated = tied(wo, gate)
        wo_xa = send(over_x, lax.dynamic_slice_in_dim(wo_gated, y_id * half, half, axis=0))
        ws = [wo, send(over_core, wo_gated)]

        os, outs = [], []
        prev = last

        def attend(j):
            o_own, o_mate, o_far, o_fm = flash(
                tab, [q_own, q_mate, q_far[j]], [(0, j), (1, j), (2, 0), (2, 1)], kvs,
                base=bases[j], work=int(work[j]), after=(prev,))
            os.append([o_own, send(over_core, o_mate), send(over_x, o_far), send(over_both, o_fm)])
            return o_own

        def project(i):
            y, b0, b1 = out_proj(os[2 * i] + os[2 * i + 1], ws, x_rows, gm, i, after=(prev,))
            for k, b in enumerate((b0, b1)):
                outs.append((y, k, b, send(over_x, b), send(over_core, b)))
            return y

        prev = attend(0)
        wo_a = tied(wo_xa, prev)
        wo_xb = send(over_y, wo_a)
        ws += [wo_a, None, send(over_core, wo_a), None]
        prev = attend(1)
        prev = attend(2)
        wo_b = tied(wo_xb, prev)
        ws[3], ws[5] = wo_b, send(over_core, wo_b)
        prev = project(0)
        prev = attend(3)

        z, pending, relay = None, None, {}

        def relay_b(j):
            here = tied(outs[j][3], prev)
            relay[j] = (here, send(over_core, here))

        relay_b(0)
        for j in range(n_run):
            y, k, b, _, b_mate = outs[j]
            keep, out = mlp([b, relay[j][0], b_mate, relay[j][1]], w_gate, w_up, w_down, after=(prev,))
            recv = send(over_core, out)
            prev = keep
            if j + 1 < n_run:
                relay_b(j + 1)
            if j == 0:
                prev = project(1)
            if pending is not None:
                prev = z = sum_run(z, *pending, j - 1, n_run, after=(prev,))
            kept = tied(keep, prev)
            prev = s_far = (kept[RUN:].astype(F32) + recv[RUN:].astype(F32)).astype(BF)
            pending = (keep, recv, send(over_x, s_far), y, k)
        z = sum_run(z, *pending, n_run - 1, n_run)
        return z[None]

    return jax.shard_map(layer, mesh=mesh,
                         in_specs=(row_spec, P(), head_cols, head_cols, head_cols, P('tp', None, None),
                                   P(), P(None, 'tp'), P(None, 'tp'), P('tp', None)),
                         out_specs=row_spec, check_vma=False)
```

time: 1440 us -> 1400 us (0.972)
  Pallas kernels: 861 us -> 782 us
  waiting for transfers between devices: 484 us -> 535 us
    pallas_call x16 -> x6, Pallas kernels: 491 us -> 428 us  [the longest x4 361 us: mlp(): pl.pallas_call(ordered(functools.partial(mlp_kernel, n_in=len(bs), tn=tn,...]
    ppermute x55, waiting for transfers between devices: 484 us -> 535 us  [send(): return lax.ppermute(v, *axis_pairs)]
    pallas_call x4, Pallas kernels: 233 us -> 216 us  [flash(): pl.pallas_call(ordered(functools.partial(flash_kernel, q_src=q_src, kv_sr...]
  transfers between devices with their start and end apart: 55 -> 55, of which waited for: 27 -> 29; matrix products, arithmetic and copies ran while one was open for 3% -> 3% of each run, Pallas kernels for 35% -> 34%
where the time goes in v3:
time: 1400 us; the launch traced here: 1390 us
  Pallas kernels  782 us (56%)
  waiting for transfers between devices  535 us (38%)
  starting transfers between devices  31.7 us (2%)
  local copies, waits for them, and re-layouts  22.8 us (2%)
  other arithmetic  20.9 us (1%)
    ppermute x55, waiting for transfers between devices, send(): return lax.ppermute(v, *axis_pairs)  535 us
    pallas_call x4, Pallas kernels, mlp(): pl.pallas_call(ordered(functools.partial(mlp_kernel, n_in=len(bs), tn=tn,...  361 us
    pallas_call x4, Pallas kernels, flash(): pl.pallas_call(ordered(functools.partial(flash_kernel, q_src=q_src, kv_sr...  216 us
    pallas_call x6, Pallas kernels, qkv(): pl.pallas_call(ordered(functools.partial(qkv_kernel, n_in=n_in, nq=nq), n...  102 us
    pallas_call x2, Pallas kernels, out_proj(): pl.pallas_call(ordered(functools.partial(out_kernel, n_w=len(ws), n_run=n...  67.4 us
    ppermute x55, starting transfers between devices, send(): return lax.ppermute(v, *axis_pairs)  31.7 us
  transfers between devices with their start and end apart: 55, of which 29 were waited for; matrix products, arithmetic and copies ran while one was open for 3% of the time, Pallas kernels for 34%

profile of v3, /device:TPU:0, one launch (start us, length us, event | category | flops | bytes accessed | tf_op | source)
XLA Modules:
  0.0 1392.9 jit_solution(10220688404952564252)
XLA Ops:
  20.1 9.5 bitcast_dynamic-update-slice_fusion
  29.6 4.8 multiply_sine_fusion
  38.3 22.5 %qkv.6 = (bf16[4,1024,256]{2,1,0:T(8,128)(2,1)}, bf16[4,2,256,256]{3,2,1,0:T(8,128)(2,1)}) custom-call(bf16[256,4096]{1,0:T(8,128)(2,1)} %norm.4.refs_2_.refs_0_, bf16[256,4096]{1,0:T(8,128)(2,1)} %norm.5.refs_2_.refs_1_, bf16[256,4096]{1,0:T(8,128)(2,1)} %norm.6.refs_2_, bf16[256,4096]{1,0:T(8,128)(2,1)} %norm.7.refs_3_, ...), custom_call_target="tpu_custom_call" | custom-call | flops 12884901888 | bytes 24117248 | tf_op jit(solution)/shard_map/qkv/pallas_call | solution.py:116
  60.9 22.7 %qkv.7 = (bf16[4,1024,256]{2,1,0:T(8,128)(2,1)}, bf16[4,2,256,256]{3,2,1,0:T(8,128)(2,1)}) custom-call(bf16[256,4096]{1,0:T(8,128)(2,1)} %collective-permute-done.refs_0_, bf16[256,4096]{1,0:T(8,128)(2,1)} %collective-permute-done.1.refs_1_, bf16[256,4096]{1,0:T(8,128)(2,1)} %collective-permute-done.2.refs_2_, ...), custom_call_target="tpu_custom_call" | custom-call | flops 12884901888 | bytes 24117248 | tf_op jit(solution)/shard_map/qkv/pallas_call | solution.py:116
  83.7 4.5 collective-permute-done.5.refs_1_
  88.1 14.1 %qkv.8 = (bf16[2,1024,256]{2,1,0:T(8,128)(2,1)}, bf16[2,2,256,256]{3,2,1,0:T(8,128)(2,1)}) custom-call(bf16[256,4096]{1,0:T(8,128)(2,1)} %collective-permute-done.4.refs_0_, bf16[256,4096]{1,0:T(8,128)(2,1)} %collective-permute-done.5.refs_1_, bf16[4096,1536]{1,0:T(8,128)(2,1)} %bitcast_dynamic-update-slice_fusion.1.refs_4_.refs_2_, ...), custom_call_target="tpu_custom_call" | custom-call | flops 6442450944 | bytes 18350080 | tf_op jit(solution)/shard_map/qkv/pallas_call | solution.py:116
  102.2 29.8 %collective-permute-done.6.refs_0_ = bf16[256,4096]{1,0:T(8,128)(2,1)} collective-permute-done((bf16[256,4096]{1,0:T(8,128)(2,1)}, bf16[256,4096]{1,0:T(8,128)(2,1)}, u32[]{:S(2)}, u32[]{:S(2)}) %collective-permute-start.6) | collective-permute-done | bytes 2097184 | tf_op jit(solution)/shard_map/ppermute | solution.py:509
  136.5 14.1 %qkv.9 = (bf16[2,1024,256]{2,1,0:T(8,128)(2,1)}, bf16[2,2,256,256]{3,2,1,0:T(8,128)(2,1)}) custom-call(bf16[256,4096]{1,0:T(8,128)(2,1)} %collective-permute-done.6.refs_0_, bf16[256,4096]{1,0:T(8,128)(2,1)} %collective-permute-done.7.refs_1_, bf16[4096,1536]{1,0:T(8,128)(2,1)} %bitcast_dynamic-update-slice_fusion.1.refs_4_.refs_2_, ...), custom_call_target="tpu_custom_call" | custom-call | flops 6442450944 | bytes 18350080 | tf_op jit(solution)/shard_map/qkv/pallas_call | solution.py:116
  150.6 29.7 %collective-permute-done.8.refs_0_ = bf16[256,4096]{1,0:T(8,128)(2,1)} collective-permute-done((bf16[256,4096]{1,0:T(8,128)(2,1)}, bf16[256,4096]{1,0:T(8,128)(2,1)}, u32[]{:S(2)}, u32[]{:S(2)}) %collective-permute-start.8) | collective-permute-done | bytes 2097184 | tf_op jit(solution)/shard_map/ppermute | solution.py:509
  184.8 14.1 %qkv.10 = (bf16[2,1024,256]{2,1,0:T(8,128)(2,1)}, bf16[2,2,256,256]{3,2,1,0:T(8,128)(2,1)}) custom-call(bf16[256,4096]{1,0:T(8,128)(2,1)} %collective-permute-done.8.refs_0_, bf16[256,4096]{1,0:T(8,128)(2,1)} %collective-permute-done.9.refs_1_, bf16[4096,1536]{1,0:T(8,128)(2,1)} %bitcast_dynamic-update-slice_fusion.1.refs_4_.refs_2_, ...), custom_call_target="tpu_custom_call" | custom-call | flops 6442450944 | bytes 18350080 | tf_op jit(solution)/shard_map/qkv/pallas_call | solution.py:116
  199.0 29.7 %collective-permute-done.10.refs_0_ = bf16[256,4096]{1,0:T(8,128)(2,1)} collective-permute-done((bf16[256,4096]{1,0:T(8,128)(2,1)}, bf16[256,4096]{1,0:T(8,128)(2,1)}, u32[]{:S(2)}, u32[]{:S(2)}) %collective-permute-start.10) | collective-permute-done | bytes 2097184 | tf_op jit(solution)/shard_map/ppermute | solution.py:509
  232.8 4.7 constant_dynamic-slice_fusion
  237.7 14.1 %qkv.11 = (bf16[2,1024,256]{2,1,0:T(8,128)(2,1)}, bf16[2,2,256,256]{3,2,1,0:T(8,128)(2,1)}) custom-call(bf16[256,4096]{1,0:T(8,128)(2,1)} %collective-permute-done.10.refs_0_, bf16[256,4096]{1,0:T(8,128)(2,1)} %collective-permute-done.11.refs_1_, bf16[4096,1536]{1,0:T(8,128)(2,1)} %bitcast_dynamic-update-slice_fusion.1.refs_4_.refs_2_, ...), custom_call_target="tpu_custom_call" | custom-call | flops 6442450944 | bytes 18350080 | tf_op jit(solution)/shard_map/qkv/pallas_call | solution.py:116
  256.6 21.0 %collective-permute-done.13.refs_11_ = bf16[4,2,256,256]{3,2,1,0:T(8,128)(2,1)} collective-permute-done((bf16[4,2,256,256]{3,2,1,0:T(8,128)(2,1)}, bf16[4,2,256,256]{3,2,1,0:T(8,128)(2,1)}, u32[]{:S(2)}, u32[]{:S(2)}) %collective-permute-start.13) | collective-permute-done | bytes 1048608 | tf_op jit(solution)/shard_map/ppermute | solution.py:509
  280.4 8.4 collective-permute-done.14.refs_12_
  288.8 11.2 collective-permute-done.15.refs_13_
  300.0 11.2 collective-permute-done.16.refs_14_
  311.2 10.8 collective-permute-done.17.refs_15_
  322.0 54.6 %flash.4 = (bf16[256,1024]{1,0:T(8,128)(2,1)}, bf16[256,1024]{1,0:T(8,128)(2,1)}, bf16[256,1024]{1,0:T(8,128)(2,1)}, bf16[256,1024]{1,0:T(8,128)(2,1)}) custom-call(s32[884]{0:T(1024)} %dynamic-slice_reduce_fusion.refs_0_, bf16[4,1024,256]{2,1,0:T(8,128)(2,1)} %get-tuple-element.70.refs_1_, bf16[4,1024,256]{2,1,0:T(8,128)(2,1)} %get-tuple-element.72.refs_2_, ...), custom_call_target="tpu_custom_call" | custom-call | flops 38654705664 | bytes 12582912 | tf_op jit(solution)/shard_map/flash/pallas_call | solution.py:255
  378.2 54.6 %flash.5 = (bf16[256,1024]{1,0:T(8,128)(2,1)}, bf16[256,1024]{1,0:T(8,128)(2,1)}, bf16[256,1024]{1,0:T(8,128)(2,1)}, bf16[256,1024]{1,0:T(8,128)(2,1)}) custom-call(s32[884]{0:T(1024)} %dynamic-slice_reduce_fusion.refs_0_, bf16[4,1024,256]{2,1,0:T(8,128)(2,1)} %get-tuple-element.70.refs_1_, bf16[4,1024,256]{2,1,0:T(8,128)(2,1)} %get-tuple-element.72.refs_2_, ...), custom_call_target="tpu_custom_call" | custom-call | flops 38654705664 | bytes 12582912 | tf_op jit(solution)/shard_map/flash/pallas_call | solution.py:255
  432.7 54.6 %flash.6 = (bf16[256,1024]{1,0:T(8,128)(2,1)}, bf16[256,1024]{1,0:T(8,128)(2,1)}, bf16[256,1024]{1,0:T(8,128)(2,1)}, bf16[256,1024]{1,0:T(8,128)(2,1)}) custom-call(s32[884]{0:T(1024)} %dynamic-slice_reduce_fusion.refs_0_, bf16[4,1024,256]{2,1,0:T(8,128)(2,1)} %get-tuple-element.70.refs_1_, bf16[4,1024,256]{2,1,0:T(8,128)(2,1)} %get-tuple-element.72.refs_2_, ...), custom_call_target="tpu_custom_call" | custom-call | flops 38654705664 | bytes 12582912 | tf_op jit(solution)/shard_map/flash/pallas_call | solution.py:255
  488.4 7.2 collective-permute-done.18.refs_1_
  496.0 7.0 collective-permute-done.19.refs_2_
  503.0 9.6 collective-permute-done.20.refs_3_
  515.9 11.8 collective-permute-done.22.refs_6_
  527.7 10.5 collective-permute-done.23.refs_7_
  538.3 33.7 %outp.2 = (bf16[512,4096]{1,0:T(8,128)(2,1)}, bf16[256,4096]{1,0:T(8,128)(2,1)}, bf16[256,4096]{1,0:T(8,128)(2,1)}) custom-call(bf16[256,1024]{1,0:T(8,128)(2,1)} %get-tuple-element.83.refs_16_.refs_0_, bf16[256,1024]{1,0:T(8,128)(2,1)} %collective-permute-done.18.refs_1_, bf16[256,1024]{1,0:T(8,128)(2,1)} %collective-permute-done.19.refs_2_, ...), custom_call_target="tpu_custom_call" | custom-call | flops 17179869184 | bytes 50331648 | tf_op jit(solution)/shard_map/outp/pallas_call | solution.py:328
  572.8 52.6 %flash.7 = (bf16[256,1024]{1,0:T(8,128)(2,1)}, bf16[256,1024]{1,0:T(8,128)(2,1)}, bf16[256,1024]{1,0:T(8,128)(2,1)}, bf16[256,1024]{1,0:T(8,128)(2,1)}) custom-call(s32[884]{0:T(1024)} %dynamic-slice_reduce_fusion.refs_0_, bf16[4,1024,256]{2,1,0:T(8,128)(2,1)} %get-tuple-element.70.refs_1_, bf16[4,1024,256]{2,1,0:T(8,128)(2,1)} %get-tuple-element.72.refs_2_, ...), custom_call_target="tpu_custom_call" | custom-call | flops 38654705664 | bytes 12582912 | tf_op jit(solution)/shard_map/flash/pallas_call | solution.py:255
  629.9 90.0 %mlp.4 = (bf16[512,4096]{1,0:T(8,128)(2,1)}, bf16[512,4096]{1,0:T(8,128)(2,1)}) custom-call(bf16[256,4096]{1,0:T(8,128)(2,1)} %get-tuple-element.97.refs_0_, bf16[256,4096]{1,0:T(8,128)(2,1)} %collective-permute-done.29.refs_1_, bf16[256,4096]{1,0:T(8,128)(2,1)} %collective-permute-done.30.refs_2_, bf16[256,4096]{1,0:T(8,128)(2,1)} %collective-permute-done.31.refs_3_, ...), custom_call_target="tpu_custom_call" | custom-call | flops 77309411328 | bytes 92274688 | tf_op jit(solution)/shard_map/mlp/pallas_call | solution.py:385
  721.9 6.3 collective-permute-done.33.refs_1_
  728.3 7.2 collective-permute-done.34.refs_2_
  737.0 8.7 collective-permute-done.35.refs_3_
  746.6 11.4 collective-permute-done.37.refs_6_
  758.0 9.6 collective-permute-done.38.refs_7_
  767.6 33.7 %outp.3 = (bf16[512,4096]{1,0:T(8,128)(2,1)}, bf16[256,4096]{1,0:T(8,128)(2,1)}, bf16[256,4096]{1,0:T(8,128)(2,1)}) custom-call(bf16[256,1024]{1,0:T(8,128)(2,1)} %get-tuple-element.95.refs_16_.refs_0_, bf16[256,1024]{1,0:T(8,128)(2,1)} %collective-permute-done.33.refs_1_, bf16[256,1024]{1,0:T(8,128)(2,1)} %collective-permute-done.34.refs_2_, ...), custom_call_target="tpu_custom_call" | custom-call | flops 17179869184 | bytes 50331648 | tf_op jit(solution)/shard_map/outp/pallas_call | solution.py:328
  805.6 90.2 %mlp.5 = (bf16[512,4096]{1,0:T(8,128)(2,1)}, bf16[512,4096]{1,0:T(8,128)(2,1)}) custom-call(bf16[256,4096]{1,0:T(8,128)(2,1)} %get-tuple-element.112.refs_0_, bf16[256,4096]{1,0:T(8,128)(2,1)} %collective-permute-done.40.refs_1_, bf16[256,4096]{1,0:T(8,128)(2,1)} %collective-permute-done.41.refs_2_, bf16[256,4096]{1,0:T(8,128)(2,1)} %collective-permute-done.42.refs_3_, ...), custom_call_target="tpu_custom_call" | custom-call | flops 77309411328 | bytes 92274688 | tf_op jit(solution)/shard_map/mlp/pallas_call | solution.py:385
  898.6 46.8 %collective-permute-done.45.refs_1_ = bf16[256,4096]{1,0:T(8,128)(2,1)} collective-permute-done((bf16[256,4096]{1,0:T(8,128)(2,1)}, bf16[256,4096]{1,0:T(8,128)(2,1)}, u32[]{:S(2)}, u32[]{:S(2)}) %collective-permute-start.45) | collective-permute-done | bytes 2097184 | tf_op jit(solution)/shard_map/ppermute | solution.py:509
  945.4 44.0 %collective-permute-done.39.refs_2_ = bf16[256,4096]{1,0:T(8,128)(2,1)} collective-permute-done((bf16[256,4096]{1,0:T(8,128)(2,1)}, bf16[256,4096]{1,0:T(8,128)(2,1)}, u32[]{:S(2)}, u32[]{:S(2)}) %collective-permute-start.39) | collective-permute-done | bytes 2097184 | tf_op jit(solution)/shard_map/ppermute | solution.py:509
  989.4 5.6 zsum.4.refs_0_
  999.3 90.1 %mlp.6 = (bf16[512,4096]{1,0:T(8,128)(2,1)}, bf16[512,4096]{1,0:T(8,128)(2,1)}) custom-call(bf16[256,4096]{1,0:T(8,128)(2,1)} %get-tuple-element.117.refs_0_, bf16[256,4096]{1,0:T(8,128)(2,1)} %collective-permute-done.45.refs_1_, bf16[256,4096]{1,0:T(8,128)(2,1)} %collective-permute-done.46.refs_2_, bf16[256,4096]{1,0:T(8,128)(2,1)} %collective-permute-done.47.refs_3_, ...), custom_call_target="tpu_custom_call" | custom-call | flops 77309411328 | bytes 92274688 | tf_op jit(solution)/shard_map/mlp/pallas_call | solution.py:385
  1091.4 46.8 %collective-permute-done.50.refs_1_ = bf16[256,4096]{1,0:T(8,128)(2,1)} collective-permute-done((bf16[256,4096]{1,0:T(8,128)(2,1)}, bf16[256,4096]{1,0:T(8,128)(2,1)}, u32[]{:S(2)}, u32[]{:S(2)}) %collective-permute-start.50) | collective-permute-done | bytes 2097184 | tf_op jit(solution)/shard_map/ppermute | solution.py:509
  1138.2 44.4 %collective-permute-done.44.refs_3_ = bf16[256,4096]{1,0:T(8,128)(2,1)} collective-permute-done((bf16[256,4096]{1,0:T(8,128)(2,1)}, bf16[256,4096]{1,0:T(8,128)(2,1)}, u32[]{:S(2)}, u32[]{:S(2)}) %collective-permute-start.44) | collective-permute-done | bytes 2097184 | tf_op jit(solution)/shard_map/ppermute | solution.py:509
  1182.7 5.6 zsum.5.refs_0_
  1192.6 90.2 %mlp.7 = (bf16[512,4096]{1,0:T(8,128)(2,1)}, bf16[512,4096]{1,0:T(8,128)(2,1)}) custom-call(bf16[256,4096]{1,0:T(8,128)(2,1)} %get-tuple-element.122.refs_0_, bf16[256,4096]{1,0:T(8,128)(2,1)} %collective-permute-done.50.refs_1_, bf16[256,4096]{1,0:T(8,128)(2,1)} %collective-permute-done.51.refs_2_, bf16[256,4096]{1,0:T(8,128)(2,1)} %collective-permute-done.52.refs_3_, ...), custom_call_target="tpu_custom_call" | custom-call | flops 77309411328 | bytes 92274688 | tf_op jit(solution)/shard_map/mlp/pallas_call | solution.py:385
  1284.4 46.9 %collective-permute-done.49.refs_3_ = bf16[256,4096]{1,0:T(8,128)(2,1)} collective-permute-done((bf16[256,4096]{1,0:T(8,128)(2,1)}, bf16[256,4096]{1,0:T(8,128)(2,1)}, u32[]{:S(2)}, u32[]{:S(2)}) %collective-permute-start.49) | collective-permute-done | bytes 2097184 | tf_op jit(solution)/shard_map/ppermute | solution.py:509
  1331.3 5.6 zsum.6.refs_0_
  1341.3 45.8 %collective-permute-done.54.refs_3_ = bf16[256,4096]{1,0:T(8,128)(2,1)} collective-permute-done((bf16[256,4096]{1,0:T(8,128)(2,1)S(1)}, bf16[256,4096]{1,0:T(8,128)(2,1)}, u32[]{:S(2)}, u32[]{:S(2)}) %collective-permute-start.54) | collective-permute-done | bytes 2097184 | tf_op jit(solution)/shard_map/ppermute | solution.py:509
  1387.1 5.6 zsum.7
  (105 shorter events, 84.7 us)
Async XLA Ops:
  4.7 78.9 %collective-permute-start.4 = (bf16[256,4096]{1,0:T(8,128)(2,1)}, bf16[256,4096]{1,0:T(8,128)(2,1)}, u32[]{:S(2)}, u32[]{:S(2)}) collective-permute-start(bf16[256,4096]{1,0:T(8,128)(2,1)} %norm.4.refs_2_.refs_0_), channel_id=1, source_target_pairs={{0,2},{1,3},{2,0},{3,1},{4,6},{5,7},{6,4},{7,5}} | collective-permute-start | bytes 6291464 | tf_op jit(solution)/shard_map/ppermute | solution.py:509
  8.0 52.8 %collective-permute-start = (bf16[256,4096]{1,0:T(8,128)(2,1)}, bf16[256,4096]{1,0:T(8,128)(2,1)}, u32[]{:S(2)}, u32[]{:S(2)}) collective-permute-start(bf16[256,4096]{1,0:T(8,128)(2,1)} %norm.4.refs_2_.refs_0_), channel_id=1, source_target_pairs={{0,1},{1,0},{2,3},{3,2},{4,5},{5,4},{6,7},{7,6}} | collective-permute-start | bytes 6291464 | tf_op jit(solution)/shard_map/ppermute | solution.py:509
  11.4 49.4 %collective-permute-start.1 = (bf16[256,4096]{1,0:T(8,128)(2,1)}, bf16[256,4096]{1,0:T(8,128)(2,1)}, u32[]{:S(2)}, u32[]{:S(2)}) collective-permute-start(bf16[256,4096]{1,0:T(8,128)(2,1)} %norm.5.refs_2_.refs_1_), channel_id=1, source_target_pairs={{0,1},{1,0},{2,3},{3,2},{4,5},{5,4},{6,7},{7,6}} | collective-permute-start | bytes 6291464 | tf_op jit(solution)/shard_map/ppermute | solution.py:509
  15.3 45.5 %collective-permute-start.2 = (bf16[256,4096]{1,0:T(8,128)(2,1)}, bf16[256,4096]{1,0:T(8,128)(2,1)}, u32[]{:S(2)}, u32[]{:S(2)}) collective-permute-start(bf16[256,4096]{1,0:T(8,128)(2,1)} %norm.6.refs_2_), channel_id=1, source_target_pairs={{0,1},{1,0},{2,3},{3,2},{4,5},{5,4},{6,7},{7,6}} | collective-permute-start | bytes 6291464 | tf_op jit(solution)/shard_map/ppermute | solution.py:509
  18.8 42.1 %collective-permute-start.3 = (bf16[256,4096]{1,0:T(8,128)(2,1)}, bf16[256,4096]{1,0:T(8,128)(2,1)}, u32[]{:S(2)}, u32[]{:S(2)}) collective-permute-start(bf16[256,4096]{1,0:T(8,128)(2,1)} %norm.7.refs_3_), channel_id=1, source_target_pairs={{0,1},{1,0},{2,3},{3,2},{4,5},{5,4},{6,7},{7,6}} | collective-permute-start | bytes 6291464 | tf_op jit(solution)/shard_map/ppermute | solution.py:509
  83.6 48.3 %collective-permute-start.6 = (bf16[256,4096]{1,0:T(8,128)(2,1)}, bf16[256,4096]{1,0:T(8,128)(2,1)}, u32[]{:S(2)}, u32[]{:S(2)}) collective-permute-start(bf16[256,4096]{1,0:T(8,128)(2,1)} %norm.5.refs_2_.refs_1_), channel_id=1, source_target_pairs={{0,2},{1,3},{2,0},{3,1},{4,6},{5,7},{6,4},{7,5}} | collective-permute-start | bytes 6291464 | tf_op jit(solution)/shard_map/ppermute | solution.py:509
  132.0 48.4 %collective-permute-start.8 = (bf16[256,4096]{1,0:T(8,128)(2,1)}, bf16[256,4096]{1,0:T(8,128)(2,1)}, u32[]{:S(2)}, u32[]{:S(2)}) collective-permute-start(bf16[256,4096]{1,0:T(8,128)(2,1)} %norm.6.refs_2_), channel_id=1, source_target_pairs={{0,2},{1,3},{2,0},{3,1},{4,6},{5,7},{6,4},{7,5}} | collective-permute-start | bytes 6291464 | tf_op jit(solution)/shard_map/ppermute | solution.py:509
  180.3 48.4 %collective-permute-start.10 = (bf16[256,4096]{1,0:T(8,128)(2,1)}, bf16[256,4096]{1,0:T(8,128)(2,1)}, u32[]{:S(2)}, u32[]{:S(2)}) collective-permute-start(bf16[256,4096]{1,0:T(8,128)(2,1)} %norm.7.refs_3_), channel_id=1, source_target_pairs={{0,2},{1,3},{2,0},{3,1},{4,6},{5,7},{6,4},{7,5}} | collective-permute-start | bytes 6291464 | tf_op jit(solution)/shard_map/ppermute | solution.py:509
  228.7 26.3 %collective-permute-start.12 = (bf16[4,2,256,256]{3,2,1,0:T(8,128)(2,1)}, bf16[4,2,256,256]{3,2,1,0:T(8,128)(2,1)}, u32[]{:S(2)}, u32[]{:S(2)}) collective-permute-start(bf16[4,2,256,256]{3,2,1,0:T(8,128)(2,1)} %get-tuple-element.71.refs_7_.refs_4_), channel_id=1, source_target_pairs={{0,4},{4,0},{1,5},{5,1},{2,6},{6,2},{3,7},{7,3}} | collective-permute-start | bytes 3145736 | tf_op jit(solution)/shard_map/ppermute | solution.py:509
  230.2 47.3 %collective-permute-start.13 = (bf16[4,2,256,256]{3,2,1,0:T(8,128)(2,1)}, bf16[4,2,256,256]{3,2,1,0:T(8,128)(2,1)}, u32[]{:S(2)}, u32[]{:S(2)}) collective-permute-start(bf16[4,2,256,256]{3,2,1,0:T(8,128)(2,1)} %get-tuple-element.73.refs_5_), channel_id=1, source_target_pairs={{0,4},{4,0},{1,5},{5,1},{2,6},{6,2},{3,7},{7,3}} | collective-permute-start | bytes 3145736 | tf_op jit(solution)/shard_map/ppermute | solution.py:509
  230.7 58.0 %collective-permute-start.14 = (bf16[2,2,256,256]{3,2,1,0:T(8,128)(2,1)}, bf16[2,2,256,256]{3,2,1,0:T(8,128)(2,1)}, u32[]{:S(2)}, u32[]{:S(2)}) collective-permute-start(bf16[2,2,256,256]{3,2,1,0:T(8,128)(2,1)} %get-tuple-element.76.refs_5_.refs_6_), channel_id=1, source_target_pairs={{0,4},{4,0},{1,5},{5,1},{2,6},{6,2},{3,7},{7,3}} | collective-permute-start | bytes 1572872 | tf_op jit(solution)/shard_map/ppermute | solution.py:509
  232.3 67.7 %collective-permute-start.15 = (bf16[2,2,256,256]{3,2,1,0:T(8,128)(2,1)}, bf16[2,2,256,256]{3,2,1,0:T(8,128)(2,1)}, u32[]{:S(2)}, u32[]{:S(2)}) collective-permute-start(bf16[2,2,256,256]{3,2,1,0:T(8,128)(2,1)} %get-tuple-element.78.refs_5_.refs_7_), channel_id=1, source_target_pairs={{0,4},{4,0},{1,5},{5,1},{2,6},{6,2},{3,7},{7,3}} | collective-permute-start | bytes 1572872 | tf_op jit(solution)/shard_map/ppermute | solution.py:509
  237.5 139.2 %collective-permute-start.25 = (bf16[512,4096]{1,0:T(8,128)(2,1)}, bf16[512,4096]{1,0:T(8,128)(2,1)}, u32[]{:S(2)}, u32[]{:S(2)}) collective-permute-start(bf16[512,4096]{1,0:T(8,128)(2,1)} %constant_dynamic-slice_fusion), channel_id=1, source_target_pairs={{0,2},{1,3},{2,0},{3,1},{4,6},{5,7},{6,4},{7,5}} | collective-permute-start | bytes 12582920 | tf_op jit(solution)/shard_map/ppermute | solution.py:509
  255.1 56.2 %collective-permute-start.16 = (bf16[2,2,256,256]{3,2,1,0:T(8,128)(2,1)}, bf16[2,2,256,256]{3,2,1,0:T(8,128)(2,1)}, u32[]{:S(2)}, u32[]{:S(2)}) collective-permute-start(bf16[2,2,256,256]{3,2,1,0:T(8,128)(2,1)} %get-tuple-element.80.refs_5_.refs_8_), channel_id=1, source_target_pairs={{0,4},{4,0},{1,5},{5,1},{2,6},{6,2},{3,7},{7,3}} | collective-permute-start | bytes 1572872 | tf_op jit(solution)/shard_map/ppermute | solution.py:509
  277.5 44.5 %collective-permute-start.17 = (bf16[2,2,256,256]{3,2,1,0:T(8,128)(2,1)}, bf16[2,2,256,256]{3,2,1,0:T(8,128)(2,1)}, u32[]{:S(2)}, u32[]{:S(2)}) collective-permute-start(bf16[2,2,256,256]{3,2,1,0:T(8,128)(2,1)} %get-tuple-element.82.refs_9_.refs_16_), channel_id=1, source_target_pairs={{0,4},{4,0},{1,5},{5,1},{2,6},{6,2},{3,7},{7,3}} | collective-permute-start | bytes 1572872 | tf_op jit(solution)/shard_map/ppermute | solution.py:509
  288.8 249.5 %collective-permute-start.24 = (bf16[1024,4096]{1,0:T(8,128)(2,1)}, bf16[1024,4096]{1,0:T(8,128)(2,1)}, u32[]{:S(2)}, u32[]{:S(2)}) collective-permute-start(bf16[1024,4096]{1,0:T(8,128)(2,1)} %bitcast.22), channel_id=1, source_target_pairs={{0,1},{1,0},{2,3},{3,2},{4,5},{5,4},{6,7},{7,6}} | collective-permute-start | bytes 25165832 | tf_op jit(solution)/shard_map/ppermute | solution.py:509
  376.6 161.7 %collective-permute-start.27 = (bf16[512,4096]{1,0:T(8,128)(2,1)}, bf16[512,4096]{1,0:T(8,128)(2,1)}, u32[]{:S(2)}, u32[]{:S(2)}) collective-permute-start(bf16[512,4096]{1,0:T(8,128)(2,1)} %collective-permute-done.25.refs_10_), channel_id=1, source_target_pairs={{0,1},{1,0},{2,3},{3,2},{4,5},{5,4},{6,7},{7,6}} | collective-permute-start | bytes 12582920 | tf_op jit(solution)/shard_map/ppermute | solution.py:509
  376.7 110.7 %collective-permute-start.26 = (bf16[512,4096]{1,0:T(8,128)(2,1)}, bf16[512,4096]{1,0:T(8,128)(2,1)}, u32[]{:S(2)}, u32[]{:S(2)}) collective-permute-start(bf16[512,4096]{1,0:T(8,128)(2,1)} %collective-permute-done.25.refs_10_), channel_id=1, source_target_pairs={{0,4},{4,0},{1,5},{5,1},{2,6},{6,2},{3,7},{7,3}} | collective-permute-start | bytes 12582920 | tf_op jit(solution)/shard_map/ppermute | solution.py:509
  487.3 50.9 %collective-permute-start.28 = (bf16[512,4096]{1,0:T(8,128)(2,1)}, bf16[512,4096]{1,0:T(8,128)(2,1)}, u32[]{:S(2)}, u32[]{:S(2)}) collective-permute-start(bf16[512,4096]{1,0:T(8,128)(2,1)} %collective-permute-done.26.refs_11_), channel_id=1, source_target_pairs={{0,1},{1,0},{2,3},{3,2},{4,5},{5,4},{6,7},{7,6}} | collective-permute-start | bytes 12582920 | tf_op jit(solution)/shard_map/ppermute | solution.py:509
  487.9 15.1 %collective-permute-start.19 = (bf16[256,1024]{1,0:T(8,128)(2,1)}, bf16[256,1024]{1,0:T(8,128)(2,1)}, u32[]{:S(2)}, u32[]{:S(2)}) collective-permute-start(bf16[256,1024]{1,0:T(8,128)(2,1)} %get-tuple-element.85), channel_id=1, source_target_pairs={{0,2},{1,3},{2,0},{3,1},{4,6},{5,7},{6,4},{7,5}} | collective-permute-start | bytes 1572872 | tf_op jit(solution)/shard_map/ppermute | solution.py:509
  495.6 17.0 %collective-permute-start.20 = (bf16[256,1024]{1,0:T(8,128)(2,1)}, bf16[256,1024]{1,0:T(8,128)(2,1)}, u32[]{:S(2)}, u32[]{:S(2)}) collective-permute-start(bf16[256,1024]{1,0:T(8,128)(2,1)} %get-tuple-element.86), channel_id=1, source_target_pairs={{0,3},{1,2},{2,1},{3,0},{4,7},{5,6},{6,5},{7,4}} | collective-permute-start | bytes 1572872 | tf_op jit(solution)/shard_map/ppermute | solution.py:509
  503.0 10.3 collective-permute-start.21
  512.6 15.1 %collective-permute-start.22 = (bf16[256,1024]{1,0:T(8,128)(2,1)}, bf16[256,1024]{1,0:T(8,128)(2,1)}, u32[]{:S(2)}, u32[]{:S(2)}) collective-permute-start(bf16[256,1024]{1,0:T(8,128)(2,1)} %get-tuple-element.90), channel_id=1, source_target_pairs={{0,2},{1,3},{2,0},{3,1},{4,6},{5,7},{6,4},{7,5}} | collective-permute-start | bytes 1572872 | tf_op jit(solution)/shard_map/ppermute | solution.py:509
  513.3 25.0 %collective-permute-start.23 = (bf16[256,1024]{1,0:T(8,128)(2,1)}, bf16[256,1024]{1,0:T(8,128)(2,1)}, u32[]{:S(2)}, u32[]{:S(2)}) collective-permute-start(bf16[256,1024]{1,0:T(8,128)(2,1)} %get-tuple-element.91), channel_id=1, source_target_pairs={{0,3},{1,2},{2,1},{3,0},{4,7},{5,6},{6,5},{7,4}} | collective-permute-start | bytes 1572872 | tf_op jit(solution)/shard_map/ppermute | solution.py:509
  572.0 55.0 %collective-permute-start.30 = (bf16[256,4096]{1,0:T(8,128)(2,1)}, bf16[256,4096]{1,0:T(8,128)(2,1)}, u32[]{:S(2)}, u32[]{:S(2)}) collective-permute-start(bf16[256,4096]{1,0:T(8,128)(2,1)} %get-tuple-element.97.refs_0_), channel_id=1, source_target_pairs={{0,1},{1,0},{2,3},{3,2},{4,5},{5,4},{6,7},{7,6}} | collective-permute-start | bytes 6291464 | tf_op jit(solution)/shard_map/ppermute | solution.py:509
  572.2 53.2 %collective-permute-start.29 = (bf16[256,4096]{1,0:T(8,128)(2,1)}, bf16[256,4096]{1,0:T(8,128)(2,1)}, u32[]{:S(2)}, u32[]{:S(2)}) collective-permute-start(bf16[256,4096]{1,0:T(8,128)(2,1)} %get-tuple-element.97.refs_0_), channel_id=1, source_target_pairs={{0,2},{1,3},{2,0},{3,1},{4,6},{5,7},{6,4},{7,5}} | collective-permute-start | bytes 6291464 | tf_op jit(solution)/shard_map/ppermute | solution.py:509
  625.5 111.5 %collective-permute-start.40 = (bf16[256,4096]{1,0:T(8,128)(2,1)}, bf16[256,4096]{1,0:T(8,128)(2,1)}, u32[]{:S(2)}, u32[]{:S(2)}) collective-permute-start(bf16[256,4096]{1,0:T(8,128)(2,1)} %get-tuple-element.112.refs_0_), channel_id=1, source_target_pairs={{0,2},{1,3},{2,0},{3,1},{4,6},{5,7},{6,4},{7,5}} | collective-permute-start | bytes 6291464 | tf_op jit(solution)/shard_map/ppermute | solution.py:509
  719.9 81.4 %collective-permute-start.32 = (bf16[512,4096]{1,0:T(8,128)(2,1)}, bf16[512,4096]{1,0:T(8,128)(2,1)}, u32[]{:S(2)}, u32[]{:S(2)}) collective-permute-start(bf16[512,4096]{1,0:T(8,128)(2,1)} %get-tuple-element.103), channel_id=1, source_target_pairs={{0,1},{1,0},{2,3},{3,2},{4,5},{5,4},{6,7},{7,6}} | collective-permute-start | bytes 12582920 | tf_op jit(solution)/shard_map/ppermute | solution.py:509
  720.5 15.1 %collective-permute-start.34 = (bf16[256,1024]{1,0:T(8,128)(2,1)}, bf16[256,1024]{1,0:T(8,128)(2,1)}, u32[]{:S(2)}, u32[]{:S(2)}) collective-permute-start(bf16[256,1024]{1,0:T(8,128)(2,1)} %get-tuple-element.105), channel_id=1, source_target_pairs={{0,2},{1,3},{2,0},{3,1},{4,6},{5,7},{6,4},{7,5}} | collective-permute-start | bytes 1572872 | tf_op jit(solution)/shard_map/ppermute | solution.py:509
  721.9 23.9 %collective-permute-start.35 = (bf16[256,1024]{1,0:T(8,128)(2,1)}, bf16[256,1024]{1,0:T(8,128)(2,1)}, u32[]{:S(2)}, u32[]{:S(2)}) collective-permute-start(bf16[256,1024]{1,0:T(8,128)(2,1)} %get-tuple-element.106), channel_id=1, source_target_pairs={{0,3},{1,2},{2,1},{3,0},{4,7},{5,6},{6,5},{7,4}} | collective-permute-start | bytes 1572872 | tf_op jit(solution)/shard_map/ppermute | solution.py:509
  728.2 18.4 %collective-permute-start.36 = (bf16[256,1024]{1,0:T(8,128)(2,1)}, bf16[256,1024]{1,0:T(8,128)(2,1)}, u32[]{:S(2)}, u32[]{:S(2)}) collective-permute-start(bf16[256,1024]{1,0:T(8,128)(2,1)} %get-tuple-element.107), channel_id=1, source_target_pairs={{0,1},{1,0},{2,3},{3,2},{4,5},{5,4},{6,7},{7,6}} | collective-permute-start | bytes 1572872 | tf_op jit(solution)/shard_map/ppermute | solution.py:509
  735.6 22.5 %collective-permute-start.37 = (bf16[256,1024]{1,0:T(8,128)(2,1)}, bf16[256,1024]{1,0:T(8,128)(2,1)}, u32[]{:S(2)}, u32[]{:S(2)}) collective-permute-start(bf16[256,1024]{1,0:T(8,128)(2,1)} %get-tuple-element.108), channel_id=1, source_target_pairs={{0,2},{1,3},{2,0},{3,1},{4,6},{5,7},{6,4},{7,5}} | collective-permute-start | bytes 1572872 | tf_op jit(solution)/shard_map/ppermute | solution.py:509
  737.0 30.6 %collective-permute-start.38 = (bf16[256,1024]{1,0:T(8,128)(2,1)}, bf16[256,1024]{1,0:T(8,128)(2,1)}, u32[]{:S(2)}, u32[]{:S(2)}) collective-permute-start(bf16[256,1024]{1,0:T(8,128)(2,1)} %get-tuple-element.109), channel_id=1, source_target_pairs={{0,3},{1,2},{2,1},{3,0},{4,7},{5,6},{6,5},{7,4}} | collective-permute-start | bytes 1572872 | tf_op jit(solution)/shard_map/ppermute | solution.py:509
  745.8 59.9 %collective-permute-start.41 = (bf16[256,4096]{1,0:T(8,128)(2,1)}, bf16[256,4096]{1,0:T(8,128)(2,1)}, u32[]{:S(2)}, u32[]{:S(2)}) collective-permute-start(bf16[256,4096]{1,0:T(8,128)(2,1)} %get-tuple-element.112.refs_0_), channel_id=1, source_target_pairs={{0,1},{1,0},{2,3},{3,2},{4,5},{5,4},{6,7},{7,6}} | collective-permute-start | bytes 6291464 | tf_op jit(solution)/shard_map/ppermute | solution.py:509
  746.6 59.0 %collective-permute-start.42 = (bf16[256,4096]{1,0:T(8,128)(2,1)}, bf16[256,4096]{1,0:T(8,128)(2,1)}, u32[]{:S(2)}, u32[]{:S(2)}) collective-permute-start(bf16[256,4096]{1,0:T(8,128)(2,1)} %collective-permute-done.40.refs_1_), channel_id=1, source_target_pairs={{0,1},{1,0},{2,3},{3,2},{4,5},{5,4},{6,7},{7,6}} | collective-permute-start | bytes 6291464 | tf_op jit(solution)/shard_map/ppermute | solution.py:509
  895.8 99.1 %collective-permute-start.43 = (bf16[512,4096]{1,0:T(8,128)(2,1)}, bf16[512,4096]{1,0:T(8,128)(2,1)}, u32[]{:S(2)}, u32[]{:S(2)}) collective-permute-start(bf16[512,4096]{1,0:T(8,128)(2,1)} %get-tuple-element.115), channel_id=1, source_target_pairs={{0,1},{1,0},{2,3},{3,2},{4,5},{5,4},{6,7},{7,6}} | collective-permute-start | bytes 12582920 | tf_op jit(solution)/shard_map/ppermute | solution.py:509
  896.5 48.8 %collective-permute-start.45 = (bf16[256,4096]{1,0:T(8,128)(2,1)}, bf16[256,4096]{1,0:T(8,128)(2,1)}, u32[]{:S(2)}, u32[]{:S(2)}) collective-permute-start(bf16[256,4096]{1,0:T(8,128)(2,1)} %get-tuple-element.117.refs_0_), channel_id=1, source_target_pairs={{0,2},{1,3},{2,0},{3,1},{4,6},{5,7},{6,4},{7,5}} | collective-permute-start | bytes 6291464 | tf_op jit(solution)/shard_map/ppermute | solution.py:509
  898.0 91.4 %collective-permute-start.39 = (bf16[256,4096]{1,0:T(8,128)(2,1)}, bf16[256,4096]{1,0:T(8,128)(2,1)}, u32[]{:S(2)}, u32[]{:S(2)}) collective-permute-start(bf16[256,4096]{1,0:T(8,128)(2,1)} %add_convert_fusion.3.refs_7_), channel_id=1, source_target_pairs={{0,2},{1,3},{2,0},{3,1},{4,6},{5,7},{6,4},{7,5}} | collective-permute-start | bytes 6291464 | tf_op jit(solution)/shard_map/ppermute | solution.py:509
  898.6 100.7 %collective-permute-start.46 = (bf16[256,4096]{1,0:T(8,128)(2,1)}, bf16[256,4096]{1,0:T(8,128)(2,1)}, u32[]{:S(2)}, u32[]{:S(2)}) collective-permute-start(bf16[256,4096]{1,0:T(8,128)(2,1)} %get-tuple-element.117.refs_0_), channel_id=1, source_target_pairs={{0,1},{1,0},{2,3},{3,2},{4,5},{5,4},{6,7},{7,6}} | collective-permute-start | bytes 6291464 | tf_op jit(solution)/shard_map/ppermute | solution.py:509
  945.4 53.9 %collective-permute-start.47 = (bf16[256,4096]{1,0:T(8,128)(2,1)}, bf16[256,4096]{1,0:T(8,128)(2,1)}, u32[]{:S(2)}, u32[]{:S(2)}) collective-permute-start(bf16[256,4096]{1,0:T(8,128)(2,1)} %collective-permute-done.45.refs_1_), channel_id=1, source_target_pairs={{0,1},{1,0},{2,3},{3,2},{4,5},{5,4},{6,7},{7,6}} | collective-permute-start | bytes 6291464 | tf_op jit(solution)/shard_map/ppermute | solution.py:509
  1089.4 98.9 %collective-permute-start.48 = (bf16[512,4096]{1,0:T(8,128)(2,1)}, bf16[512,4096]{1,0:T(8,128)(2,1)}, u32[]{:S(2)}, u32[]{:S(2)}) collective-permute-start(bf16[512,4096]{1,0:T(8,128)(2,1)} %get-tuple-element.120), channel_id=1, source_target_pairs={{0,1},{1,0},{2,3},{3,2},{4,5},{5,4},{6,7},{7,6}} | collective-permute-start | bytes 12582920 | tf_op jit(solution)/shard_map/ppermute | solution.py:509
  1089.4 48.8 %collective-permute-start.50 = (bf16[256,4096]{1,0:T(8,128)(2,1)}, bf16[256,4096]{1,0:T(8,128)(2,1)}, u32[]{:S(2)}, u32[]{:S(2)}) collective-permute-start(bf16[256,4096]{1,0:T(8,128)(2,1)} %get-tuple-element.122.refs_0_), channel_id=1, source_target_pairs={{0,2},{1,3},{2,0},{3,1},{4,6},{5,7},{6,4},{7,5}} | collective-permute-start | bytes 6291464 | tf_op jit(solution)/shard_map/ppermute | solution.py:509
  1090.9 91.8 %collective-permute-start.44 = (bf16[256,4096]{1,0:T(8,128)(2,1)}, bf16[256,4096]{1,0:T(8,128)(2,1)}, u32[]{:S(2)}, u32[]{:S(2)}) collective-permute-start(bf16[256,4096]{1,0:T(8,128)(2,1)} %add_convert_fusion.2.refs_7_), channel_id=1, source_target_pairs={{0,2},{1,3},{2,0},{3,1},{4,6},{5,7},{6,4},{7,5}} | collective-permute-start | bytes 6291464 | tf_op jit(solution)/shard_map/ppermute | solution.py:509
  1091.4 101.2 %collective-permute-start.51 = (bf16[256,4096]{1,0:T(8,128)(2,1)}, bf16[256,4096]{1,0:T(8,128)(2,1)}, u32[]{:S(2)}, u32[]{:S(2)}) collective-permute-start(bf16[256,4096]{1,0:T(8,128)(2,1)} %get-tuple-element.122.refs_0_), channel_id=1, source_target_pairs={{0,1},{1,0},{2,3},{3,2},{4,5},{5,4},{6,7},{7,6}} | collective-permute-start | bytes 6291464 | tf_op jit(solution)/shard_map/ppermute | solution.py:509
  1138.2 54.4 %collective-permute-start.52 = (bf16[256,4096]{1,0:T(8,128)(2,1)}, bf16[256,4096]{1,0:T(8,128)(2,1)}, u32[]{:S(2)}, u32[]{:S(2)}) collective-permute-start(bf16[256,4096]{1,0:T(8,128)(2,1)} %collective-permute-done.50.refs_1_), channel_id=1, source_target_pairs={{0,1},{1,0},{2,3},{3,2},{4,5},{5,4},{6,7},{7,6}} | collective-permute-start | bytes 6291464 | tf_op jit(solution)/shard_map/ppermute | solution.py:509
  1282.9 54.0 %collective-permute-start.53 = (bf16[512,4096]{1,0:T(8,128)(2,1)}, bf16[512,4096]{1,0:T(8,128)(2,1)}, u32[]{:S(2)}, u32[]{:S(2)}) collective-permute-start(bf16[512,4096]{1,0:T(8,128)(2,1)} %get-tuple-element.125), channel_id=1, source_target_pairs={{0,1},{1,0},{2,3},{3,2},{4,5},{5,4},{6,7},{7,6}} | collective-permute-start | bytes 12582920 | tf_op jit(solution)/shard_map/ppermute | solution.py:509
  1282.9 48.3 %collective-permute-start.49 = (bf16[256,4096]{1,0:T(8,128)(2,1)}, bf16[256,4096]{1,0:T(8,128)(2,1)}, u32[]{:S(2)}, u32[]{:S(2)}) collective-permute-start(bf16[256,4096]{1,0:T(8,128)(2,1)} %add_convert_fusion.1.refs_7_), channel_id=1, source_target_pairs={{0,2},{1,3},{2,0},{3,1},{4,6},{5,7},{6,4},{7,5}} | collective-permute-start | bytes 6291464 | tf_op jit(solution)/shard_map/ppermute | solution.py:509
  1339.8 47.3 %collective-permute-start.54 = (bf16[256,4096]{1,0:T(8,128)(2,1)S(1)}, bf16[256,4096]{1,0:T(8,128)(2,1)}, u32[]{:S(2)}, u32[]{:S(2)}) collective-permute-start(bf16[256,4096]{1,0:T(8,128)(2,1)S(1)} %add_convert_fusion), channel_id=1, source_target_pairs={{0,2},{1,3},{2,0},{3,1},{4,6},{5,7},{6,4},{7,5}} | collective-permute-start | bytes 6291464 | tf_op jit(solution)/shard_map/ppermute | solution.py:509
  (9 other events, 64.1 us)

commit v4 on v3

v4 whole, which is shorter than its diff:
```python
import functools
import math
import jax
import jax.numpy as jnp
import numpy as np
from jax import lax
from jax.experimental import pallas as pl
from jax.experimental.pallas import tpu as pltpu
from jax.sharding import PartitionSpec as P

NORM_EPS = 1e-5
ROPE_THETA = 500000.0
HD = 128
RUN = 256
NEG = -1e30
FAR = 1 << 29
LOG2E = math.log2(math.e)
DN = (((1,), (0,)), ((), ()))
VMEM = 67043328
BF = jnp.bfloat16
F32 = jnp.float32
ANY = pl.BlockSpec(memory_space=pltpu.HBM)


def params(n):
    return pltpu.CompilerParams(dimension_semantics=("arbitrary",) * n, vmem_limit_bytes=VMEM)


def rope_tables(positions):
    half = HD // 2
    inv_freq = ROPE_THETA ** (-2.0 * jnp.arange(half, dtype=F32) / HD)
    angles = inv_freq[:, None] * positions.astype(F32)[..., None, :]
    return jnp.cos(angles), jnp.sin(angles)


def norm_rows(rows, gain):
    f = rows.astype(F32)
    mean_sq = jnp.mean(f * f, axis=-1, keepdims=True)
    return (f * lax.rsqrt(mean_sq + NORM_EPS) * gain.astype(F32)).astype(BF)


def ordered(kernel, n_in, after):
    n = len(after)
    return lambda *refs: kernel(*refs[:n_in], *refs[n_in + n:])


def load_all(pairs, sem):
    copies = [pltpu.make_async_copy(src, dst, sem.at[i]) for i, (src, dst) in enumerate(pairs)]
    for cp in copies:
        cp.start()
    for cp in copies:
        cp.wait()


def norm_kernel(x_ref, g_ref, o_ref):
    o_ref[...] = norm_rows(x_ref[...], g_ref[...])


def norm_run(x_rows, gain, j, after=(), tile=128):
    dim = x_rows.shape[1]
    per = RUN // tile
    return pl.pallas_call(
        ordered(norm_kernel, 2, after), grid=(per,),
        in_specs=[pl.BlockSpec((tile, dim), lambda i: (j * per + i, 0)), pl.BlockSpec((1, dim), lambda i: (0, 0))]
        + [ANY] * len(after),
        out_specs=pl.BlockSpec((tile, dim), lambda i: (i, 0)),
        out_shape=jax.ShapeDtypeStruct((RUN, dim), BF),
        name="norm", compiler_params=params(1),
        cost_estimate=pl.CostEstimate(flops=8 * RUN * dim, transcendentals=0, bytes_accessed=4 * RUN * dim),
    )(x_rows, gain, *after)


def qkv_kernel(*refs, n_in, n_q, group):
    a_refs = refs[:n_in]
    w_ref, cos_ref, sin_ref, q_ref, kv_ref, a_scr, sem = refs[n_in:]
    n = pl.program_id(0)
    heads = w_ref.shape[1] // HD

    @pl.when(n == 0)
    def _():
        for k, r in enumerate(a_refs):
            pltpu.make_async_copy(r, a_scr.at[pl.ds(k * RUN, RUN), :], sem.at[k]).start()

    def rope(f, i):
        f = f.astype(BF).astype(F32)
        lo, hi, cos, sin = f[:HD // 2], f[HD // 2:], cos_ref[i], sin_ref[i]
        return jnp.concatenate([lo * cos - hi * sin, hi * cos + lo * sin], axis=0)

    def one(k, carry):
        @pl.when(n == 0)
        def _():
            for i in range(group):
                rows = pl.ds(pl.multiple_of((k * group + i) * RUN, RUN), RUN)
                pltpu.make_async_copy(a_scr.at[rows, :], a_scr.at[rows, :], sem.at[k * group + i]).wait()

        rows = pl.ds(pl.multiple_of(k * group * RUN, group * RUN), group * RUN)
        r = jnp.dot(a_scr[rows, :], w_ref[...], preferred_element_type=F32)

        def piece(i, h):
            return r[i * RUN:(i + 1) * RUN, h * HD:(h + 1) * HD].T

        @pl.when(n < n_q)
        def _():
            for i in range(group):
                for h in range(heads):
                    q_ref[k * group + i, h * HD:(h + 1) * HD, :] = rope(piece(i, h), k * group + i).astype(BF)

        @pl.when(n == n_q)
        def _():
            for i in range(group):
                for h in range(heads // 2):
                    kv_ref[k * group + i, 0, :, h * HD:(h + 1) * HD] = rope(piece(i, h), k * group + i).T.astype(BF)
                    kv_ref[k * group + i, 1, h * HD:(h + 1) * HD, :] = piece(i, h + heads // 2).astype(BF)

        return carry

    lax.fori_loop(0, n_in // group, one, 0)


def qkv(rows, w_all, tables, after=(), group=2):
    n_in = len(rows)
    dim = w_all.shape[0]
    tn = 512
    n_q = w_all.shape[1] // tn - 1
    (cos, sin), first_run = tables
    at = first_run // n_in
    tab = pl.BlockSpec((n_in, HD // 2, RUN), lambda n: (at, 0, 0))
    return pl.pallas_call(
        ordered(functools.partial(qkv_kernel, n_in=n_in, n_q=n_q, group=group), n_in + 3, after),
        grid=(n_q + 1,),
        in_specs=[ANY] * n_in + [pl.BlockSpec((dim, tn), lambda n: (0, n)), tab, tab] + [ANY] * len(after),
        out_specs=[pl.BlockSpec((n_in, tn, RUN), lambda n: (0, jnp.minimum(n, n_q - 1), 0)),
                   pl.BlockSpec((n_in, 2, 256, 256), lambda n: (0, 0, 0, 0))],
        out_shape=[jax.ShapeDtypeStruct((n_in, n_q * tn, RUN), BF), jax.ShapeDtypeStruct((n_in, 2, 256, 256), BF)],
        scratch_shapes=[pltpu.VMEM((n_in * RUN, dim), BF), pltpu.SemaphoreType.DMA((n_in,))],
        name="qkv", compiler_params=params(1),
        cost_estimate=pl.CostEstimate(flops=2 * n_in * RUN * w_all.size, transcendentals=0,
                                      bytes_accessed=2 * (n_in * RUN * dim + w_all.size)),
    )(*rows, w_all, cos, sin, *after)


BLK = 12
MASK0, MASK1, LAST, FIRST, CARRY = 1, 2, 4, 8, 16
ST = HD + 16


def flash_kernel(tab_ref, *refs, q_src, kv_src, n_q, n_kv, st_src, n_st, base, G, n_tiles, n_heads, final):
    qs, kvs, sts = refs[:n_q], refs[n_q:n_q + n_kv], refs[n_q + n_kv:n_q + n_kv + n_st]
    n_out = n_tiles if final else 1
    at = n_q + n_kv + n_st
    outs = refs[at:at + n_out]
    q_scr, kv_scr, o_scr, st_scr, s_scr, mb_scr, acc_scr, m_scr, l_scr, q_sem, kv_sem, o_sem, st_sem = refs[at + n_out:]
    T = RUN
    c = (HD ** -0.5) * LOG2E
    n_blocks = tab_ref[base]
    carried = base + 1 + n_tiles
    row0 = base + 1 + 2 * n_tiles

    q_copies = [pltpu.make_async_copy(qs[a].at[i], q_scr.at[t], q_sem.at[t]) for t, (a, i) in enumerate(q_src)]
    kv_copies = [pltpu.make_async_copy(kvs[a].at[i], kv_scr.at[r], kv_sem.at[r]) for r, (a, i) in enumerate(kv_src)]
    for cp in q_copies:
        cp.start()
    for t, i in enumerate(st_src):
        if i is not None:
            @pl.when(tab_ref[carried + t] != 0)
            def _():
                pltpu.make_async_copy(sts[0].at[i], st_scr.at[t], st_sem.at[t]).start()
    for cp in kv_copies:
        cp.start()
    for cp in q_copies:
        cp.wait()

    def block(i):
        g = lax.div(i, n_blocks)
        return row0 + BLK * (i - g * n_blocks), g

    def arrived(have, need):
        def one(r, carry):
            pltpu.make_async_copy(kv_scr.at[r], kv_scr.at[r], kv_sem.at[r]).wait()
            return carry

        lax.fori_loop(have, need, one, 0)
        return jnp.maximum(have, need)

    def put(s, slot):
        s_scr[slot] = s
        mb = jnp.max(s.reshape(2 * RUN // 8, 8, T), axis=0)
        for r in (4, 2, 1):
            mb = jnp.maximum(mb, pltpu.roll(mb, r, 0))
        mb_scr[slot] = mb

    def stage_a(row, g, it, h):
        col = pl.multiple_of(g * HD, HD)
        qt = q_scr[tab_ref[row], pl.ds(pl.multiple_of((g * G + h) * HD, HD), HD), :]
        put(jnp.concatenate([lax.dot_general(kv_scr[tab_ref[row + 3 + 2 * it + k], 0, :, pl.ds(col, HD)], qt, DN,
                                             preferred_element_type=F32) for k in range(2)], axis=0), it * G + h)

    def stage_b(row, g, it, h):
        slot = it * G + h
        col = pl.multiple_of(g * HD, HD)
        m_prev = m_scr[h]
        m_new = jnp.maximum(m_prev, mb_scr[slot])
        m_scr[h] = m_new
        m_c = m_new * c
        p = jnp.exp2(s_scr[slot].reshape(2 * RUN // 8, 8, T) * c - m_c[None])
        alpha = jnp.exp2(m_prev * c - m_c)
        l_scr[h] = l_scr[h] * alpha + jnp.sum(p, axis=0)
        pb = p.reshape(2 * RUN, T).astype(BF)
        pv = sum(lax.dot_general(kv_scr[tab_ref[row + 3 + 2 * it + k], 1, pl.ds(col, HD), :], pb[k * RUN:(k + 1) * RUN], DN,
                                 preferred_element_type=F32) for k in range(2))
        acc_scr[h] = (acc_scr[h].reshape(HD // 8, 8, T) * alpha[None]).reshape(HD, T) + pv

    def mask_item(row, it):
        key = lax.broadcasted_iota(jnp.int32, (RUN, T), 0)
        qry = lax.broadcasted_iota(jnp.int32, (RUN, T), 1) + tab_ref[base + 1 + tab_ref[row]]
        mask = jnp.concatenate([key + tab_ref[row + 7 + 2 * it + k] <= qry for k in range(2)], axis=0)
        for h in range(G):
            put(jnp.where(mask, s_scr[it * G + h], NEG), it * G + h)

    def finish(tile, g, get):
        for h in range(G):
            acc, l = get(h)
            o_scr[tile, :, pl.ds(pl.multiple_of((g * G + h) * HD, HD), HD)] = (acc / jnp.sum(l, axis=0, keepdims=True)).T.astype(BF)

        @pl.when(g == n_heads - 1)
        def _():
            for k in range(n_tiles):
                @pl.when(tile == k)
                def _():
                    pltpu.make_async_copy(o_scr.at[k], outs[k], o_sem.at[k]).start()

    if final and n_st:
        def idle(i, carry):
            tile, g = lax.div(i, n_heads), lax.rem(i, n_heads)

            @pl.when(tab_ref[carried + tile] == 2)
            def _():
                @pl.when(g == 0)
                def _():
                    pltpu.make_async_copy(st_scr.at[tile], st_scr.at[tile], st_sem.at[tile]).wait()

                finish(tile, g, lambda h: (st_scr[tile, g, h, :HD, :], st_scr[tile, g, h, HD + 8:, :]))

            return carry

        lax.fori_loop(0, n_tiles * n_heads, idle, 0)

    row, g = block(0)
    have = arrived(0, tab_ref[row + 2])
    for it in range(2):
        for h in range(G):
            stage_a(row, g, it, h)

    def body(i, have):
        row, g = block(i)
        nrow, ng = block(jnp.minimum(i + 1, n_heads * n_blocks - 1))
        have = arrived(have, tab_ref[nrow + 2])
        flags = tab_ref[row + 1]
        tile = tab_ref[row]

        @pl.when((flags & (FIRST | CARRY)) == FIRST)
        def _():
            acc_scr[...] = jnp.zeros_like(acc_scr)
            l_scr[...] = jnp.zeros_like(l_scr)
            m_scr[...] = jnp.full_like(m_scr, NEG)

        if n_st:
            @pl.when((flags & (FIRST | CARRY)) == (FIRST | CARRY))
            def _():
                @pl.when(g == 0)
                def _():
                    pltpu.make_async_copy(st_scr.at[tile], st_scr.at[tile], st_sem.at[tile]).wait()

                for h in range(G):
                    acc_scr[h] = st_scr[tile, g, h, :HD, :]
                    m_scr[h] = st_scr[tile, g, h, HD:HD + 8, :]
                    l_scr[h] = st_scr[tile, g, h, HD + 8:, :]

        @pl.when((flags & MASK0) != 0)
        def _():
            mask_item(row, 0)

        @pl.when((flags & MASK1) != 0)
        def _():
            mask_item(row, 1)

        for it in range(2):
            for h in range(G):
                stage_b(row, g, it, h)
                stage_a(nrow, ng, it, h)

        @pl.when((flags & LAST) != 0)
        def _():
            if final:
                finish(tile, g, lambda h: (acc_scr[h], l_scr[h]))
            else:
                for h in range(G):
                    st_scr[tile, g, h, :HD, :] = acc_scr[h]
                    st_scr[tile, g, h, HD:HD + 8, :] = m_scr[h]
                    st_scr[tile, g, h, HD + 8:, :] = l_scr[h]

                @pl.when(g == n_heads - 1)
                def _():
                    pltpu.make_async_copy(st_scr.at[tile], outs[0].at[tile], o_sem.at[tile]).start()

        return have

    have = lax.fori_loop(0, n_heads * n_blocks, body, have)
    arrived(have, len(kv_src))
    if final:
        for k in range(n_tiles):
            pltpu.make_async_copy(o_scr.at[k], outs[k], o_sem.at[k]).wait()
    else:
        def wait_out(i, carry):
            row = row0 + BLK * i

            @pl.when((tab_ref[row + 1] & LAST) != 0)
            def _():
                t = tab_ref[row]
                pltpu.make_async_copy(st_scr.at[t], st_scr.at[t], o_sem.at[t]).wait()

            return carry

        lax.fori_loop(0, n_blocks, wait_out, 0)


def flash(tab, qs, q_src, kvs, *, base, work, st=None, st_src=None, st_tiles=None, after=()):
    nq = qs[0].shape[1]
    n_heads = 2
    G = nq // HD // n_heads
    n_tiles = len(q_src)
    final = st_tiles is None
    kv_src = [(a, i) for a, kv in enumerate(kvs) for i in range(kv.shape[0])]
    n_runs = len(kv_src)
    slots = 2 * G
    sts = () if st is None else (st,)
    n_in = 1 + len(qs) + len(kvs) + len(sts)
    state = (n_heads, G, ST, RUN)
    has_st = not final or sts
    return pl.pallas_call(
        ordered(functools.partial(flash_kernel, q_src=q_src, kv_src=kv_src, n_q=len(qs), n_kv=len(kvs),
                                  st_src=st_src or [None] * n_tiles, n_st=len(sts), base=base, G=G, n_tiles=n_tiles,
                                  n_heads=n_heads, final=final), n_in, after),
        grid_spec=pltpu.PrefetchScalarGridSpec(
            num_scalar_prefetch=1, grid=(),
            in_specs=[ANY] * (n_in - 1 + len(after)),
            out_specs=[ANY] * n_tiles if final else [ANY],
            scratch_shapes=[pltpu.VMEM((n_tiles, nq, RUN), BF),
                            pltpu.VMEM((n_runs, 2, 256, 256), BF),
                            pltpu.VMEM((n_tiles if final else 1, RUN, nq), BF),
                            pltpu.VMEM((n_tiles if has_st else 1, *state), F32),
                            pltpu.VMEM((slots, 2 * RUN, RUN), F32),
                            pltpu.VMEM((slots, 8, RUN), F32),
                            pltpu.VMEM((G, HD, RUN), F32),
                            pltpu.VMEM((G, 8, RUN), F32),
                            pltpu.VMEM((G, 8, RUN), F32),
                            pltpu.SemaphoreType.DMA((n_tiles,)),
                            pltpu.SemaphoreType.DMA((n_runs,)),
                            pltpu.SemaphoreType.DMA((n_tiles,)),
                            pltpu.SemaphoreType.DMA((n_tiles,))]),
        out_shape=[jax.ShapeDtypeStruct((RUN, nq), BF)] * n_tiles if final
        else [jax.ShapeDtypeStruct((st_tiles, *state), F32)],
        input_output_aliases={n_in - 1: 0} if sts and not final else {},
        name="flash" if final else "flash_part", compiler_params=pltpu.CompilerParams(vmem_limit_bytes=VMEM),
        cost_estimate=pl.CostEstimate(flops=8 * work * RUN * RUN * nq, transcendentals=work * RUN * RUN * nq // HD,
                                      bytes_accessed=n_runs * 2 * 256 * 256 * 2 + 4 * n_tiles * RUN * nq),
    )(tab, *qs, *kvs, *sts, *after)


def out_kernel(*refs, blocks, n_w):
    o_refs, w_refs = refs[:4], refs[4:4 + n_w]
    x_ref, g_ref, y_ref, b_ref, o_scr, w_scr, acc_scr, o_sem, w_sem = refs[4 + n_w:]
    width = o_refs[0].shape[1]
    half = width // 2
    n_slots = w_scr.shape[0]

    def fetch(k):
        for i, parts in enumerate(blocks):
            @pl.when(k == i)
            def _():
                at = 0
                for a, r0, n in parts:
                    pltpu.make_async_copy(w_refs[a].at[pl.ds(r0, n), :], w_scr.at[i % n_slots, pl.ds(at, n), :],
                                          w_sem.at[i % n_slots]).start()
                    at += n

    for i in range(n_slots - 1):
        fetch(jnp.int32(i))
    mine = lax.axis_index('cp')
    pairs = [(o_refs[0], o_scr.at[:, pl.ds(0, width)]), (o_refs[1], o_scr.at[:, pl.ds(width, width)])]
    for k in range(2, 4):
        for p, part in enumerate((mine, 1 - mine)):
            pairs.append((o_refs[k].at[:, pl.ds(pl.multiple_of(part * half, half), half)],
                          o_scr.at[:, pl.ds(k * width + p * half, half)]))
    load_all(pairs, o_sem)
    acc_scr[...] = jnp.zeros_like(acc_scr)

    def one(k, carry):
        fetch(k + n_slots - 1)
        slot = lax.rem(k, n_slots)
        pltpu.make_async_copy(w_scr.at[slot], w_scr.at[slot], w_sem.at[slot]).wait()
        acc_scr[...] += jnp.dot(o_scr[:, pl.ds(pl.multiple_of(k * half, half), half)], w_scr[slot], preferred_element_type=F32)
        return carry

    lax.fori_loop(0, len(blocks), one, 0)

    def rows32(i, carry):
        rows = pl.ds(pl.multiple_of(i * 32, 32), 32)
        y = (x_ref[rows, :].astype(F32) + acc_scr[rows, :].astype(BF).astype(F32)).astype(BF)
        y_ref[rows, :] = y
        b_ref[rows, :] = norm_rows(y, g_ref[...])
        return carry

    lax.fori_loop(0, RUN // 32, rows32, 0)


def out_proj(os, ws, blocks, x_rows, gain, j, after=()):
    dim = x_rows.shape[1]
    width = os[0].shape[1]
    one = lambda s: pl.BlockSpec((RUN, dim), lambda i: (s, 0))
    n_after = len(after)
    return pl.pallas_call(
        ordered(functools.partial(out_kernel, blocks=blocks, n_w=len(ws)), 6 + len(ws), after),
        grid=(1,),
        in_specs=[ANY] * (4 + len(ws)) + [one(j), pl.BlockSpec((1, dim), lambda i: (0, 0))] + [ANY] * n_after,
        out_specs=[one(0)] * 2,
        out_shape=[jax.ShapeDtypeStruct((RUN, dim), BF)] * 2,
        scratch_shapes=[pltpu.VMEM((RUN, 4 * width), BF), pltpu.VMEM((3, width // 2, dim), BF), pltpu.VMEM((RUN, dim), F32),
                        pltpu.SemaphoreType.DMA((6,)), pltpu.SemaphoreType.DMA((3,))],
        name="outp", compiler_params=params(1),
        cost_estimate=pl.CostEstimate(flops=8 * RUN * width * dim, transcendentals=0,
                                      bytes_accessed=8 * width * dim + 8 * RUN * dim),
    )(*os, *ws, x_rows, gain, *after)


def mlp_kernel(*refs, n_in, tn, nk):
    b_refs = refs[:n_in]
    wg_ref, wu_ref, wd_ref, keep_ref, send_ref, b_scr, u_scr, sem = refs[n_in:]
    i = pl.program_id(0)

    def gated(rows, cols):
        b = b_scr[rows, :]
        gate = jnp.dot(b, wg_ref[...], preferred_element_type=F32)
        up = jnp.dot(b, wu_ref[...], preferred_element_type=F32)
        u_scr[rows, cols] = (jax.nn.silu(gate) * up).astype(BF)

    @pl.when(i == 0)
    def _():
        copies = [pltpu.make_async_copy(r, b_scr.at[pl.ds(k * RUN, RUN), :], sem.at[k]) for k, r in enumerate(b_refs)]
        for cp in copies:
            cp.start()

        def one(k, carry):
            rows = pl.ds(pl.multiple_of(k * RUN, RUN), RUN)
            pltpu.make_async_copy(b_scr.at[rows, :], b_scr.at[rows, :], sem.at[k]).wait()
            gated(rows, pl.ds(0, tn))
            return carry

        lax.fori_loop(0, n_in, one, 0)

    @pl.when((i > 0) & (i < nk))
    def _():
        gated(slice(None), pl.ds(pl.multiple_of(i * tn, tn), tn))

    @pl.when(i >= nk)
    def _():
        d = jnp.dot(u_scr[...], wd_ref[...], preferred_element_type=F32).astype(BF)
        half = d.shape[0] // 2
        keep_ref[...] = d[:half]
        send_ref[...] = d[half:]


def mlp(bs, wg, wu, wd, after=(), tn=256, td=256):
    rows, dim = RUN * len(bs), bs[0].shape[1]
    ffn = wg.shape[1]
    nk, nd = ffn // tn, dim // td
    up = lambda i: (0, jnp.minimum(i, nk - 1))
    dn = lambda i: (0, jnp.maximum(i - nk, 0))
    return pl.pallas_call(
        ordered(functools.partial(mlp_kernel, n_in=len(bs), tn=tn, nk=nk), len(bs) + 3, after),
        grid=(nk + nd,),
        in_specs=[ANY] * len(bs) + [pl.BlockSpec((dim, tn), up), pl.BlockSpec((dim, tn), up), pl.BlockSpec((ffn, td), dn)]
        + [ANY] * len(after),
        out_specs=[pl.BlockSpec((rows // 2, td), dn)] * 2,
        out_shape=[jax.ShapeDtypeStruct((rows // 2, dim), BF)] * 2,
        scratch_shapes=[pltpu.VMEM((rows, dim), BF), pltpu.VMEM((rows, ffn), BF), pltpu.SemaphoreType.DMA((len(bs),))],
        name="mlp", compiler_params=params(1),
        cost_estimate=pl.CostEstimate(flops=6 * rows * dim * ffn, transcendentals=rows * ffn,
                                      bytes_accessed=6 * dim * ffn + 4 * rows * dim),
    )(*bs, wg, wu, wd, *after)


def sum_kernel(*refs):
    p_ref, r_ref, t_ref, y_ref, z_ref = refs[-5:]
    total = p_ref[...].astype(F32) + r_ref[...].astype(F32) + t_ref[...].astype(F32)
    z_ref[...] = (y_ref[...].astype(F32) + total.astype(BF).astype(F32)).astype(BF)


def sum_run(z, keep, recv, far, y, j, n_runs, after=(), tile=64):
    dim = y.shape[1]
    per = RUN // tile
    spec = pl.BlockSpec((tile, dim), lambda i: (i, 0))
    prev = () if z is None else (z,)
    return pl.pallas_call(
        ordered(sum_kernel, len(prev) + 4, after), grid=(per,),
        in_specs=[ANY] * len(prev) + [spec] * 4 + [ANY] * len(after),
        out_specs=pl.BlockSpec((tile, dim), lambda i: (j * per + i, 0)),
        out_shape=jax.ShapeDtypeStruct((n_runs * RUN, dim), BF),
        input_output_aliases={0: 0} if prev else {},
        name="zsum", compiler_params=params(1),
        cost_estimate=pl.CostEstimate(flops=6 * RUN * dim, transcendentals=0, bytes_accessed=10 * RUN * dim),
    )(*prev, keep, recv, far, y, *after)


def run_positions(xi, ci, y, cps, piece):
    def start(x, c):
        return (y if x == 0 else 2 * cps - 1 - y) * piece + c * (piece // 2)

    per = piece // 2 // RUN
    out = [start(xi, ci) + RUN * j for j in range(per)] + [start(xi, 1 - ci) + RUN * j for j in range(per)]
    for j in range(per):
        out += [start(1 - xi, ci) + RUN * j, start(1 - xi, 1 - ci) + RUN * j]
    return out


def block_list(tile, ids, pos, diag):
    runs = [(r, pos[r]) for r in ids]
    if diag is not None:
        n_tail = (len(runs) % 4) + 1
        tail = [(diag, pos[diag])] + runs[len(runs) - (n_tail - 1):]
        runs = runs[:len(runs) - (n_tail - 1)]
    else:
        n_tail = len(runs) % 4
        tail = runs[len(runs) - n_tail:]
        runs = runs[:len(runs) - n_tail]
    blocks = [[0, runs[i:i + 4]] for i in range(0, len(runs), 4)]
    if tail:
        full = tail + [(tail[0][0], FAR)] * (4 - len(tail))
        flags = (MASK0 if diag is not None or len(tail) < 2 else 0) | (MASK1 if len(tail) < 4 else 0)
        blocks.append([flags, full])
    blocks[-1][0] |= LAST
    blocks[0][0] |= FIRST
    return [[tile, flags, 0] + [r for r, _ in four] + [p for _, p in four] + [0] for flags, four in blocks]


def call_table(tiles, pos, pairs, carry, idle):
    rows, most = [], 0
    carry = [c if pairs[t][0] or pairs[t][1] else idle for t, c in enumerate(carry)]
    for t, tile in enumerate(tiles):
        ids, own = pairs[t]
        if ids or own:
            mine = block_list(t, ids, pos, tile if own else None)
            mine[0][1] |= CARRY if carry[t] else 0
            rows += mine
    for row in rows:
        most = max(most, max(row[3:7]) + 1)
        row[2] = most
    return [len(rows)] + [pos[t] for t in tiles] + carry + [v for row in rows for v in row], len(rows)


def work_tables(cps, piece):
    per = piece // 2 // RUN
    early = 2 * per + 2
    later = early + 4
    stage = lambda r: 0 if r < early else 1 if r < later else 2
    calls = [(0, list(range(early))), (1, list(range(later)))]
    calls += [(2, [j, per + j, 2 * per + 2 * j, 2 * per + 2 * j + 1]) for j in range(per)]
    tabs, all_runs, sizes = [], [], []
    for y in range(cps):
        for xi in range(2):
            for ci in range(2):
                mine = run_positions(xi, ci, y, cps, piece)
                pos = mine + run_positions(xi, ci, 1 - y, cps, piece)
                all_runs.append(mine)
                tabs.append([])
                sizes.append([])
                for now, tiles in calls:
                    pairs, carry = [], []
                    for t in tiles:
                        seen = [r for r in range(len(pos)) if pos[r] < pos[t]]
                        pairs.append(([r for r in seen if max(stage(r), stage(t)) == now], stage(t) == now))
                        carry.append(int(stage(t) < now))
                    tab, n = call_table(tiles, pos, pairs, carry, 2 if now == 2 else 0)
                    tabs[-1].append(tab)
                    sizes[-1].append(n)
    widths = [max(len(t[k]) for t in tabs) for k in range(len(calls))]
    flat = [[v for k, t in enumerate(tab) for v in t + [0] * (widths[k] - len(t))] for tab in tabs]
    bases = [sum(widths[:k]) for k in range(len(calls))]
    return np.array(flat, np.int32), np.array(all_runs, np.int32), bases, np.array(sizes).max(0) * 4


def solution(mesh):
    cps = mesh.shape['cp']
    row_spec = P('dp', ('cp', 'tp'), None)
    head_cols = P(None, 'tp', None)
    n_tp = mesh.shape['tp']

    over_core, over_x, over_both = (('tp', [(t, t ^ k) for t in range(n_tp)]) for k in (1, 2, 3))
    over_y = ('cp', [(i, i ^ 1) for i in range(cps)])

    def layer(x, g_attn, w_q, w_k, w_v, w_o, g_mlp, w_gate, w_up, w_down):
        x_rows = x[0]
        dim = x_rows.shape[1]
        n_run = x_rows.shape[0] // RUN
        piece = 2 * x_rows.shape[0]
        t_id, y_id = lax.axis_index('tp'), lax.axis_index('cp')
        np_tab, np_runs, bases, work = work_tables(cps, piece)
        dev = y_id * n_tp + t_id
        tab = lax.dynamic_index_in_dim(jnp.asarray(np_tab), dev, 0, keepdims=False)
        order = list(range(2 * n_run)) + [2 * n_run + i for i in (2, 3, 4, 5, 0, 1, 6, 7)]
        run_pos = lax.dynamic_index_in_dim(jnp.asarray(np_runs[:, order]), dev, 0, keepdims=False)

        def tied(v, *others):
            return lax.optimization_barrier((v, *others))[0]

        def send(axis_pairs, v):
            return lax.ppermute(v, *axis_pairs)

        ga, gm = g_attn.reshape(1, dim), g_mlp.reshape(1, dim)
        own = []
        for j in range(n_run):
            own.append(norm_run(x_rows, ga, j, after=own[-1:]))
        far = [send(over_x, own[j]) for j in range(n_run)]
        mate = [send(over_core, own[j]) for j in range(n_run)]

        w_all = jnp.concatenate([tied(w, own[-1]).reshape(dim, -1) for w in (w_q, w_k, w_v)], axis=1)
        tables = rope_tables(tied(run_pos, own[-1])[:, None] + jnp.arange(RUN, dtype=jnp.int32)[None, :])

        def relayed(j, after):
            here = tied(far[j], after)
            return [here, send(over_core, here)]

        q_own, kv_own = qkv(own, w_all, (tables, 0))
        q_mate, kv_mate = qkv(mate, w_all, (tables, n_run), after=(kv_own,))
        q_a, kv_a = qkv(relayed(0, kv_mate), w_all, (tables, 2 * n_run + 4), after=(kv_mate,))

        wo = w_o.reshape(-1, dim)
        half = wo.shape[0] // 2
        n_piece = 4
        rows = half // n_piece
        wo_gated = tied(wo, kv_a)
        wo_x = [send(over_x, lax.dynamic_slice_in_dim(wo_gated, y_id * half + p * rows, rows, axis=0))
                for p in range(n_piece)]
        wo_c = send(over_core, wo_gated)
        early = relayed(1, kv_a)

        tile = lambda a, n: [(a, i) for i in range(n)]
        tiles = tile(0, n_run) + tile(1, n_run) + tile(2, 2)
        st, = flash(tab, [q_own, q_mate, q_a], tiles, [kv_own, kv_mate, kv_a], base=bases[0],
                   work=int(work[0]), st_tiles=len(tiles) + 4)
        q_b, kv_b = qkv(early + relayed(2, st), w_all, (tables, 2 * n_run), after=(st,))
        st, = flash(tab, [q_own, q_mate, q_a, q_b], tiles + tile(3, 4), [kv_own, kv_mate, kv_a, kv_b],
                   base=bases[1], work=int(work[1]), st=st, st_src=list(range(len(tiles))) + [None] * 4,
                   st_tiles=len(tiles) + 4)
        q_c, kv_c = qkv(relayed(3, st), w_all, (tables, 2 * n_run + 6), after=(st,))
        kvs = [kv_own, kv_mate, kv_a, kv_b, kv_c]
        kvs = kvs + [send(over_y, kv) for kv in kvs]
        q_far = [(q_a, 0), (q_b, 0), (q_b, 2), (q_c, 0)]

        os, outs, prev = [], [], kv_c
        wo_a, wo_ya, wo_yb = {}, {}, {}

        def forward_w(p):
            here = tied(wo_x[p], prev)
            wo_ya[p] = (here, send(over_core, here))
            wo_a[p] = send(over_y, here)

        def relay_w(p):
            here = tied(wo_a[p], prev)
            wo_yb[p] = (here, send(over_core, here))

        def attend(j):
            q, at = q_far[j]
            held = 2 * n_run + 2 * j
            carried = [j, n_run + j] + ([held, held + 1] if j + 1 < n_run else [None, None])
            o_own, o_mate, o_far, o_fm = flash(
                tab, [q_own, q_mate, q], [(0, j), (1, j), (2, at), (2, at + 1)], kvs,
                base=bases[2 + j], work=int(work[2 + j]), st=st, st_src=carried, after=(prev,))
            os.append([o_own, send(over_core, o_mate), send(over_x, o_far), send(over_both, o_fm)])
            return o_own

        def project(j):
            ws = [wo, wo_c]
            blocks = [[(0, 0, half)], [(0, half, half)], [(1, 0, half)], [(1, half, half)]]
            for k in range(2):
                for held in (wo_ya, wo_yb):
                    blocks.append([(len(ws) + p, 0, rows) for p in range(n_piece)])
                    ws += [held[p][k] for p in range(n_piece)]
            y, b = out_proj(os[j], ws, blocks, x_rows, gm, j, after=(prev,))
            outs.append((y, b, send(over_x, b), send(over_core, b)))
            return y

        forward_w(0)
        prev = attend(0)
        forward_w(1)
        relay_w(0)
        prev = attend(1)
        forward_w(2)
        forward_w(3)
        relay_w(1)
        prev = attend(2)
        relay_w(2)
        relay_w(3)
        prev = project(0)
        prev = attend(3)
        prev = project(1)

        z, sums, relay = None, [], {}

        def relay_b(j):
            here = tied(outs[j][2], prev)
            relay[j] = (here, send(over_core, here))

        def finish(j):
            return sum_run(z, *sums[j], j, n_run, after=() if prev is z else (prev,))

        relay_b(0)
        for j in range(n_run):
            y, b, _, b_mate = outs[j]
            keep, out = mlp([b, relay[j][0], b_mate, relay[j][1]], w_gate, w_up, w_down, after=(prev,))
            recv = send(over_core, out)
            prev = keep
            if j + 1 < n_run:
                relay_b(j + 1)
            if j + 2 < n_run:
                prev = project(j + 2)
            else:
                prev = z = finish(j - 2)
            kept = tied(keep, prev)
            prev = s_far = (kept[RUN:].astype(F32) + recv[RUN:].astype(F32)).astype(BF)
            sums.append((keep, recv, send(over_x, s_far), y))
        for j in range(n_run - 2, n_run):
            prev = z = finish(j)
        return z[None]

    return jax.shard_map(layer, mesh=mesh,
                         in_specs=(row_spec, P(), head_cols, head_cols, head_cols, P('tp', None, None),
                                   P(), P(None, 'tp'), P(None, 'tp'), P('tp', None)),
                         out_specs=row_spec, check_vma=False)
```

time: 1400 us -> 1440 us (1.029)
  Pallas kernels: 782 us -> 820 us
  starting transfers between devices: 31.7 us -> 68.8 us
  waiting for transfers between devices: 535 us -> 500 us
    ppermute x55 -> x66, starting transfers between devices: 31.7 us -> 68.8 us  [send(): return lax.ppermute(v, *axis_pairs)]
    ppermute x55 -> x66, waiting for transfers between devices: 535 us -> 500 us  [send(): return lax.ppermute(v, *axis_pairs)]
    pallas_call x4 -> x6, Pallas kernels: 216 us -> 247 us  [flash(): pl.pallas_call(ordered(functools.partial(flash_kernel, q_src=q_src, kv_sr...]
    pallas_call x8 -> x9, Pallas kernels: 169 us -> 176 us  [the longest x5 96.4 us: qkv(): pl.pallas_call(ordered(functools.partial(qkv_kernel, n_in=n_in, n_q=n_q,...]
  transfers between devices with their start and end apart: 55 -> 66, of which waited for: 29 -> 26; matrix products, arithmetic and copies ran while one was open for 3% -> 3% of each run, Pallas kernels for 34% -> 31%
where the time goes in v4:
time: 1440 us; the launch traced here: 1430 us
  Pallas kernels  820 us (57%)
  waiting for transfers between devices  500 us (35%)
  starting transfers between devices  68.8 us (5%)
  other arithmetic  22.4 us (2%)
  local copies, waits for them, and re-layouts  22.3 us (2%)
    ppermute x66, waiting for transfers between devices, send(): return lax.ppermute(v, *axis_pairs)  500 us
    pallas_call x4, Pallas kernels, mlp(): pl.pallas_call(ordered(functools.partial(mlp_kernel, n_in=len(bs), tn=tn,...  360 us
    pallas_call x6, Pallas kernels, flash(): pl.pallas_call(ordered(functools.partial(flash_kernel, q_src=q_src, kv_sr...  247 us
    pallas_call x5, Pallas kernels, qkv(): pl.pallas_call(ordered(functools.partial(qkv_kernel, n_in=n_in, n_q=n_q,...  96.4 us
    pallas_call x4, Pallas kernels, out_proj(): pl.pallas_call(ordered(functools.partial(out_kernel, blocks=blocks, n_w=l...  79.7 us
    ppermute x66, starting transfers between devices, send(): return lax.ppermute(v, *axis_pairs)  68.8 us
  transfers between devices with their start and end apart: 66, of which 26 were waited for; matrix products, arithmetic and copies ran while one was open for 3% of the time, Pallas kernels for 31%

profile of v4, /device:TPU:0, one launch (start us, length us, event | category | flops | bytes accessed | tf_op | source)
XLA Modules:
  0.0 1433.9 jit_solution(8220458006394448505)
XLA Ops:
  19.0 9.4 bitcast_dynamic-update-slice_fusion
  31.1 4.8 multiply_sine_fusion
  38.0 22.7 %qkv.5 = (bf16[4,1024,256]{2,1,0:T(8,128)(2,1)}, bf16[4,2,256,256]{3,2,1,0:T(8,128)(2,1)}) custom-call(bf16[256,4096]{1,0:T(8,128)(2,1)} %norm.4.refs_2_.refs_0_, bf16[256,4096]{1,0:T(8,128)(2,1)} %norm.5.refs_2_.refs_1_, bf16[256,4096]{1,0:T(8,128)(2,1)} %norm.6.refs_2_, bf16[256,4096]{1,0:T(8,128)(2,1)} %norm.7.refs_3_, ...), custom_call_target="tpu_custom_call" | custom-call | flops 12884901888 | bytes 20971520 | tf_op jit(solution)/shard_map/qkv/pallas_call | solution.py:128
  60.8 22.7 %qkv.6 = (bf16[4,1024,256]{2,1,0:T(8,128)(2,1)}, bf16[4,2,256,256]{3,2,1,0:T(8,128)(2,1)}) custom-call(bf16[256,4096]{1,0:T(8,128)(2,1)} %collective-permute-done.refs_0_, bf16[256,4096]{1,0:T(8,128)(2,1)} %collective-permute-done.1.refs_1_, bf16[256,4096]{1,0:T(8,128)(2,1)} %collective-permute-done.2.refs_2_, ...), custom_call_target="tpu_custom_call" | custom-call | flops 12884901888 | bytes 20971520 | tf_op jit(solution)/shard_map/qkv/pallas_call | solution.py:128
  88.0 14.3 qkv.7
  102.3 58.4 %flash_part.2.refs_7_.refs_9_ = f32[14,2,4,144,256]{4,3,2,1,0:T(8,128)} custom-call(s32[1058]{0:T(1024)} %dynamic-slice_reduce_fusion.refs_0_, bf16[4,1024,256]{2,1,0:T(8,128)(2,1)} %get-tuple-element.76.refs_1_, bf16[4,1024,256]{2,1,0:T(8,128)(2,1)} %get-tuple-element.78.refs_2_, bf16[2,1024,256]{2,1,0:T(8,128)(2,1)} %get-tuple-element.81.refs_3_, ...), custom_call_target="tpu_custom_call" | custom-call | flops 38654705664 | bytes 13107200 | tf_op jit(solution)/shard_map/flash_part/pallas_call | solution.py:340
  161.0 15.8 %collective-permute-done.6.refs_0_ = bf16[256,4096]{1,0:T(8,128)(2,1)} collective-permute-done((bf16[256,4096]{1,0:T(8,128)(2,1)}, bf16[256,4096]{1,0:T(8,128)(2,1)}, u32[]{:S(2)}, u32[]{:S(2)}) %collective-permute-start.6) | collective-permute-done | bytes 2097184 | tf_op jit(solution)/shard_map/ppermute | solution.py:617
  181.3 22.6 %qkv.8 = (bf16[4,1024,256]{2,1,0:T(8,128)(2,1)}, bf16[4,2,256,256]{3,2,1,0:T(8,128)(2,1)}) custom-call(bf16[256,4096]{1,0:T(8,128)(2,1)} %collective-permute-done.6.refs_0_, bf16[256,4096]{1,0:T(8,128)(2,1)} %collective-permute-done.7.refs_1_, bf16[256,4096]{1,0:T(8,128)(2,1)} %collective-permute-done.8.refs_2_, ...), custom_call_target="tpu_custom_call" | custom-call | flops 12884901888 | bytes 20971520 | tf_op jit(solution)/shard_map/qkv/pallas_call | solution.py:128
  204.0 47.5 %flash_part.3.refs_5_.refs_14_ = f32[14,2,4,144,256]{4,3,2,1,0:T(8,128)} custom-call(s32[1058]{0:T(1024)} %dynamic-slice_reduce_fusion.refs_0_, bf16[4,1024,256]{2,1,0:T(8,128)(2,1)} %get-tuple-element.76.refs_1_, bf16[4,1024,256]{2,1,0:T(8,128)(2,1)} %get-tuple-element.78.refs_2_, ...), custom_call_target="tpu_custom_call", output_to_operand_aliasing={{}: (9, {})} | custom-call | flops 32212254720 | bytes 18350080 | tf_op jit(solution)/shard_map/flash_part/pallas_call | solution.py:340
  264.3 14.1 qkv.9
  278.4 5.6 collective-permute-done.21.refs_6_
  286.6 22.5 %collective-permute-done.13.refs_10_ = bf16[4,2,256,256]{3,2,1,0:T(8,128)(2,1)} collective-permute-done((bf16[4,2,256,256]{3,2,1,0:T(8,128)(2,1)}, bf16[4,2,256,256]{3,2,1,0:T(8,128)(2,1)}, u32[]{:S(2)}, u32[]{:S(2)}) %collective-permute-start.13) | collective-permute-done | bytes 1048608 | tf_op jit(solution)/shard_map/ppermute | solution.py:617
  309.0 11.2 collective-permute-done.14.refs_11_
  320.3 22.5 %collective-permute-done.15.refs_12_ = bf16[4,2,256,256]{3,2,1,0:T(8,128)(2,1)} collective-permute-done((bf16[4,2,256,256]{3,2,1,0:T(8,128)(2,1)}, bf16[4,2,256,256]{3,2,1,0:T(8,128)(2,1)}, u32[]{:S(2)}, u32[]{:S(2)}) %collective-permute-start.15) | collective-permute-done | bytes 1048608 | tf_op jit(solution)/shard_map/ppermute | solution.py:617
  342.7 10.1 collective-permute-done.16.refs_13_
  354.6 32.1 %flash.4 = (bf16[256,1024]{1,0:T(8,128)(2,1)}, bf16[256,1024]{1,0:T(8,128)(2,1)}, bf16[256,1024]{1,0:T(8,128)(2,1)}, bf16[256,1024]{1,0:T(8,128)(2,1)}) custom-call(s32[1058]{0:T(1024)} %dynamic-slice_reduce_fusion.refs_0_, bf16[4,1024,256]{2,1,0:T(8,128)(2,1)} %get-tuple-element.76.refs_1_, bf16[4,1024,256]{2,1,0:T(8,128)(2,1)} %get-tuple-element.78.refs_2_, ...), custom_call_target="tpu_custom_call" | custom-call | flops 23622320128 | bytes 12582912 | tf_op jit(solution)/shard_map/flash/pallas_call | solution.py:340
  386.8 31.8 %flash.5 = (bf16[256,1024]{1,0:T(8,128)(2,1)}, bf16[256,1024]{1,0:T(8,128)(2,1)}, bf16[256,1024]{1,0:T(8,128)(2,1)}, bf16[256,1024]{1,0:T(8,128)(2,1)}) custom-call(s32[1058]{0:T(1024)} %dynamic-slice_reduce_fusion.refs_0_, bf16[4,1024,256]{2,1,0:T(8,128)(2,1)} %get-tuple-element.76.refs_1_, bf16[4,1024,256]{2,1,0:T(8,128)(2,1)} %get-tuple-element.78.refs_2_, ...), custom_call_target="tpu_custom_call" | custom-call | flops 23622320128 | bytes 12582912 | tf_op jit(solution)/shard_map/flash/pallas_call | solution.py:340
  421.1 12.2 collective-permute-start.18
  433.3 12.6 collective-permute-done.18.refs_2_
  446.4 21.0 %collective-permute-done.27.refs_12_ = bf16[128,4096]{1,0:T(8,128)(2,1)} collective-permute-done((bf16[128,4096]{1,0:T(8,128)(2,1)}, bf16[128,4096]{1,0:T(8,128)(2,1)}, u32[]{:S(2)}, u32[]{:S(2)}) %collective-permute-start.27) | collective-permute-done | bytes 1048608 | tf_op jit(solution)/shard_map/ppermute | solution.py:617
  467.4 22.0 %collective-permute-done.26.refs_11_ = bf16[128,4096]{1,0:T(8,128)(2,1)} collective-permute-done((bf16[128,4096]{1,0:T(8,128)(2,1)}, bf16[128,4096]{1,0:T(8,128)(2,1)}, u32[]{:S(2)}, u32[]{:S(2)}) %collective-permute-start.26) | collective-permute-done | bytes 1048608 | tf_op jit(solution)/shard_map/ppermute | solution.py:617
  489.4 11.8 collective-permute-start.19
  501.2 31.7 %flash.6 = (bf16[256,1024]{1,0:T(8,128)(2,1)}, bf16[256,1024]{1,0:T(8,128)(2,1)}, bf16[256,1024]{1,0:T(8,128)(2,1)}, bf16[256,1024]{1,0:T(8,128)(2,1)}) custom-call(s32[1058]{0:T(1024)} %dynamic-slice_reduce_fusion.refs_0_, bf16[4,1024,256]{2,1,0:T(8,128)(2,1)} %get-tuple-element.76.refs_1_, bf16[4,1024,256]{2,1,0:T(8,128)(2,1)} %get-tuple-element.78.refs_2_, ...), custom_call_target="tpu_custom_call" | custom-call | flops 23622320128 | bytes 12582912 | tf_op jit(solution)/shard_map/flash/pallas_call | solution.py:340
  537.5 6.1 collective-permute-start.39
  545.1 19.9 %outp.4 = (bf16[256,4096]{1,0:T(8,128)(2,1)}, bf16[256,4096]{1,0:T(8,128)(2,1)}) custom-call(bf16[256,1024]{1,0:T(8,128)(2,1)} %get-tuple-element.89.refs_15_.refs_0_, bf16[256,1024]{1,0:T(8,128)(2,1)} %collective-permute-done.17.refs_1_, bf16[256,1024]{1,0:T(8,128)(2,1)} %collective-permute-done.18.refs_2_, ...), custom_call_target="tpu_custom_call" | custom-call | flops 8589934592 | bytes 41943040 | tf_op jit(solution)/shard_map/outp/pallas_call | solution.py:422
  566.6 45.6 %flash.7 = (bf16[256,1024]{1,0:T(8,128)(2,1)}, bf16[256,1024]{1,0:T(8,128)(2,1)}, bf16[256,1024]{1,0:T(8,128)(2,1)}, bf16[256,1024]{1,0:T(8,128)(2,1)}) custom-call(s32[1058]{0:T(1024)} %dynamic-slice_reduce_fusion.refs_0_, bf16[4,1024,256]{2,1,0:T(8,128)(2,1)} %get-tuple-element.76.refs_1_, bf16[4,1024,256]{2,1,0:T(8,128)(2,1)} %get-tuple-element.78.refs_2_, ...), custom_call_target="tpu_custom_call" | custom-call | flops 32212254720 | bytes 12582912 | tf_op jit(solution)/shard_map/flash/pallas_call | solution.py:340
  612.3 20.0 %outp.5 = (bf16[256,4096]{1,0:T(8,128)(2,1)}, bf16[256,4096]{1,0:T(8,128)(2,1)}) custom-call(bf16[256,1024]{1,0:T(8,128)(2,1)} %get-tuple-element.96.refs_15_.refs_0_, bf16[256,1024]{1,0:T(8,128)(2,1)} %collective-permute-done.38.refs_1_, bf16[256,1024]{1,0:T(8,128)(2,1)} %collective-permute-done.39.refs_2_, ...), custom_call_target="tpu_custom_call" | custom-call | flops 8589934592 | bytes 41943040 | tf_op jit(solution)/shard_map/outp/pallas_call | solution.py:422
  636.9 90.0 %mlp.4 = (bf16[512,4096]{1,0:T(8,128)(2,1)}, bf16[512,4096]{1,0:T(8,128)(2,1)}) custom-call(bf16[256,4096]{1,0:T(8,128)(2,1)} %get-tuple-element.104.refs_0_, bf16[256,4096]{1,0:T(8,128)(2,1)} %collective-permute-done.37.refs_1_, bf16[256,4096]{1,0:T(8,128)(2,1)} %collective-permute-done.41.refs_2_, bf16[256,4096]{1,0:T(8,128)(2,1)} %collective-permute-done.42.refs_3_, ...), custom_call_target="tpu_custom_call" | custom-call | flops 77309411328 | bytes 92274688 | tf_op jit(solution)/shard_map/mlp/pallas_call | solution.py:479
  729.4 46.7 %collective-permute-done.49.refs_1_ = bf16[256,4096]{1,0:T(8,128)(2,1)} collective-permute-done((bf16[256,4096]{1,0:T(8,128)(2,1)}, bf16[256,4096]{1,0:T(8,128)(2,1)}, u32[]{:S(2)}, u32[]{:S(2)}) %collective-permute-start.49) | collective-permute-done | bytes 2097184 | tf_op jit(solution)/shard_map/ppermute | solution.py:617
  776.6 10.7 collective-permute-done.45.refs_2_
  787.3 9.6 collective-permute-done.46.refs_3_
  796.9 19.9 %outp.6 = (bf16[256,4096]{1,0:T(8,128)(2,1)}, bf16[256,4096]{1,0:T(8,128)(2,1)}) custom-call(bf16[256,1024]{1,0:T(8,128)(2,1)} %get-tuple-element.101.refs_24_.refs_0_, bf16[256,1024]{1,0:T(8,128)(2,1)} %collective-permute-done.44.refs_1_, bf16[256,1024]{1,0:T(8,128)(2,1)} %collective-permute-done.45.refs_2_, ...), custom_call_target="tpu_custom_call" | custom-call | flops 8589934592 | bytes 41943040 | tf_op jit(solution)/shard_map/outp/pallas_call | solution.py:422
  821.2 90.2 %mlp.5 = (bf16[512,4096]{1,0:T(8,128)(2,1)}, bf16[512,4096]{1,0:T(8,128)(2,1)}) custom-call(bf16[256,4096]{1,0:T(8,128)(2,1)} %get-tuple-element.121.refs_0_, bf16[256,4096]{1,0:T(8,128)(2,1)} %collective-permute-done.49.refs_1_, bf16[256,4096]{1,0:T(8,128)(2,1)} %collective-permute-done.50.refs_2_, bf16[256,4096]{1,0:T(8,128)(2,1)} %collective-permute-done.51.refs_3_, ...), custom_call_target="tpu_custom_call" | custom-call | flops 77309411328 | bytes 92274688 | tf_op jit(solution)/shard_map/mlp/pallas_call | solution.py:479
  914.2 46.7 %collective-permute-done.48.refs_1_ = bf16[256,4096]{1,0:T(8,128)(2,1)} collective-permute-done((bf16[256,4096]{1,0:T(8,128)(2,1)}, bf16[256,4096]{1,0:T(8,128)(2,1)}, u32[]{:S(2)}, u32[]{:S(2)}) %collective-permute-start.48) | collective-permute-done | bytes 2097184 | tf_op jit(solution)/shard_map/ppermute | solution.py:617
  961.4 10.7 collective-permute-done.55.refs_2_
  972.1 9.4 collective-permute-done.56.refs_3_
  981.5 19.9 %outp.7 = (bf16[256,4096]{1,0:T(8,128)(2,1)}, bf16[256,4096]{1,0:T(8,128)(2,1)}) custom-call(bf16[256,1024]{1,0:T(8,128)(2,1)} %get-tuple-element.110.refs_24_.refs_0_, bf16[256,1024]{1,0:T(8,128)(2,1)} %collective-permute-done.54.refs_1_, bf16[256,1024]{1,0:T(8,128)(2,1)} %collective-permute-done.55.refs_2_, ...), custom_call_target="tpu_custom_call" | custom-call | flops 8589934592 | bytes 41943040 | tf_op jit(solution)/shard_map/outp/pallas_call | solution.py:422
  1005.7 90.3 %mlp.6 = (bf16[512,4096]{1,0:T(8,128)(2,1)}, bf16[512,4096]{1,0:T(8,128)(2,1)}) custom-call(bf16[256,4096]{1,0:T(8,128)(2,1)} %get-tuple-element.120.refs_0_, bf16[256,4096]{1,0:T(8,128)(2,1)} %collective-permute-done.48.refs_1_, bf16[256,4096]{1,0:T(8,128)(2,1)} %collective-permute-done.52.refs_2_, bf16[256,4096]{1,0:T(8,128)(2,1)} %collective-permute-done.53.refs_3_, ...), custom_call_target="tpu_custom_call" | custom-call | flops 77309411328 | bytes 92274688 | tf_op jit(solution)/shard_map/mlp/pallas_call | solution.py:479
  1098.8 46.8 %collective-permute-done.59.refs_1_ = bf16[256,4096]{1,0:T(8,128)(2,1)} collective-permute-done((bf16[256,4096]{1,0:T(8,128)(2,1)}, bf16[256,4096]{1,0:T(8,128)(2,1)}, u32[]{:S(2)}, u32[]{:S(2)}) %collective-permute-start.59) | collective-permute-done | bytes 2097184 | tf_op jit(solution)/shard_map/ppermute | solution.py:617
  1145.6 44.0 %collective-permute-done.47.refs_2_ = bf16[256,4096]{1,0:T(8,128)(2,1)} collective-permute-done((bf16[256,4096]{1,0:T(8,128)(2,1)}, bf16[256,4096]{1,0:T(8,128)(2,1)}, u32[]{:S(2)}, u32[]{:S(2)}) %collective-permute-start.47) | collective-permute-done | bytes 2097184 | tf_op jit(solution)/shard_map/ppermute | solution.py:617
  1189.6 5.6 zsum.4.refs_0_
  1199.6 90.0 %mlp.7 = (bf16[512,4096]{1,0:T(8,128)(2,1)}, bf16[512,4096]{1,0:T(8,128)(2,1)}) custom-call(bf16[256,4096]{1,0:T(8,128)(2,1)} %get-tuple-element.132.refs_0_, bf16[256,4096]{1,0:T(8,128)(2,1)} %collective-permute-done.59.refs_1_, bf16[256,4096]{1,0:T(8,128)(2,1)} %collective-permute-done.60.refs_2_, bf16[256,4096]{1,0:T(8,128)(2,1)} %collective-permute-done.61.refs_3_, ...), custom_call_target="tpu_custom_call" | custom-call | flops 77309411328 | bytes 92274688 | tf_op jit(solution)/shard_map/mlp/pallas_call | solution.py:479
  1291.7 46.8 %collective-permute-done.58.refs_3_ = bf16[256,4096]{1,0:T(8,128)(2,1)} collective-permute-done((bf16[256,4096]{1,0:T(8,128)(2,1)}, bf16[256,4096]{1,0:T(8,128)(2,1)}, u32[]{:S(2)}, u32[]{:S(2)}) %collective-permute-start.58) | collective-permute-done | bytes 2097184 | tf_op jit(solution)/shard_map/ppermute | solution.py:617
  1338.5 5.6 zsum.5.refs_0_
  1348.8 34.7 %collective-permute-done.63.refs_3_ = bf16[256,4096]{1,0:T(8,128)(2,1)} collective-permute-done((bf16[256,4096]{1,0:T(8,128)(2,1)}, bf16[256,4096]{1,0:T(8,128)(2,1)}, u32[]{:S(2)}, u32[]{:S(2)}) %collective-permute-start.63) | collective-permute-done | bytes 2097184 | tf_op jit(solution)/shard_map/ppermute | solution.py:617
  1383.5 5.6 zsum.6.refs_0_
  1389.0 38.9 %collective-permute-done.65.refs_3_ = bf16[256,4096]{1,0:T(8,128)(2,1)} collective-permute-done((bf16[256,4096]{1,0:T(8,128)(2,1)}, bf16[256,4096]{1,0:T(8,128)(2,1)}, u32[]{:S(2)}, u32[]{:S(2)}) %collective-permute-start.65) | collective-permute-done | bytes 2097184 | tf_op jit(solution)/shard_map/ppermute | solution.py:617
  1427.9 5.6 zsum.7
  (130 shorter events, 94.8 us)
Async XLA Ops:
  4.7 56.0 %collective-permute-start = (bf16[256,4096]{1,0:T(8,128)(2,1)}, bf16[256,4096]{1,0:T(8,128)(2,1)}, u32[]{:S(2)}, u32[]{:S(2)}) collective-permute-start(bf16[256,4096]{1,0:T(8,128)(2,1)} %norm.4.refs_2_.refs_0_), channel_id=1, source_target_pairs={{0,1},{1,0},{2,3},{3,2},{4,5},{5,4},{6,7},{7,6}} | collective-permute-start | bytes 6291464 | tf_op jit(solution)/shard_map/ppermute | solution.py:617
  5.5 77.9 %collective-permute-start.4 = (bf16[256,4096]{1,0:T(8,128)(2,1)}, bf16[256,4096]{1,0:T(8,128)(2,1)}, u32[]{:S(2)}, u32[]{:S(2)}) collective-permute-start(bf16[256,4096]{1,0:T(8,128)(2,1)} %norm.4.refs_2_.refs_0_), channel_id=1, source_target_pairs={{0,2},{1,3},{2,0},{3,1},{4,6},{5,7},{6,4},{7,5}} | collective-permute-start | bytes 6291464 | tf_op jit(solution)/shard_map/ppermute | solution.py:617
  11.5 49.3 %collective-permute-start.1 = (bf16[256,4096]{1,0:T(8,128)(2,1)}, bf16[256,4096]{1,0:T(8,128)(2,1)}, u32[]{:S(2)}, u32[]{:S(2)}) collective-permute-start(bf16[256,4096]{1,0:T(8,128)(2,1)} %norm.5.refs_2_.refs_1_), channel_id=1, source_target_pairs={{0,1},{1,0},{2,3},{3,2},{4,5},{5,4},{6,7},{7,6}} | collective-permute-start | bytes 6291464 | tf_op jit(solution)/shard_map/ppermute | solution.py:617
  15.1 45.6 %collective-permute-start.2 = (bf16[256,4096]{1,0:T(8,128)(2,1)}, bf16[256,4096]{1,0:T(8,128)(2,1)}, u32[]{:S(2)}, u32[]{:S(2)}) collective-permute-start(bf16[256,4096]{1,0:T(8,128)(2,1)} %norm.6.refs_2_), channel_id=1, source_target_pairs={{0,1},{1,0},{2,3},{3,2},{4,5},{5,4},{6,7},{7,6}} | collective-permute-start | bytes 6291464 | tf_op jit(solution)/shard_map/ppermute | solution.py:617
  83.8 76.9 %collective-permute-start.8 = (bf16[256,4096]{1,0:T(8,128)(2,1)}, bf16[256,4096]{1,0:T(8,128)(2,1)}, u32[]{:S(2)}, u32[]{:S(2)}) collective-permute-start(bf16[256,4096]{1,0:T(8,128)(2,1)} %norm.6.refs_2_), channel_id=1, source_target_pairs={{0,2},{1,3},{2,0},{3,1},{4,6},{5,7},{6,4},{7,5}} | collective-permute-start | bytes 6291464 | tf_op jit(solution)/shard_map/ppermute | solution.py:617
  83.8 93.0 %collective-permute-start.6 = (bf16[256,4096]{1,0:T(8,128)(2,1)}, bf16[256,4096]{1,0:T(8,128)(2,1)}, u32[]{:S(2)}, u32[]{:S(2)}) collective-permute-start(bf16[256,4096]{1,0:T(8,128)(2,1)} %norm.5.refs_2_.refs_1_), channel_id=1, source_target_pairs={{0,2},{1,3},{2,0},{3,1},{4,6},{5,7},{6,4},{7,5}} | collective-permute-start | bytes 6291464 | tf_op jit(solution)/shard_map/ppermute | solution.py:617
  176.8 74.7 %collective-permute-start.10 = (bf16[256,4096]{1,0:T(8,128)(2,1)}, bf16[256,4096]{1,0:T(8,128)(2,1)}, u32[]{:S(2)}, u32[]{:S(2)}) collective-permute-start(bf16[256,4096]{1,0:T(8,128)(2,1)} %norm.7.refs_3_), channel_id=1, source_target_pairs={{0,2},{1,3},{2,0},{3,1},{4,6},{5,7},{6,4},{7,5}} | collective-permute-start | bytes 6291464 | tf_op jit(solution)/shard_map/ppermute | solution.py:617
  262.0 47.0 %collective-permute-start.13 = (bf16[4,2,256,256]{3,2,1,0:T(8,128)(2,1)}, bf16[4,2,256,256]{3,2,1,0:T(8,128)(2,1)}, u32[]{:S(2)}, u32[]{:S(2)}) collective-permute-start(bf16[4,2,256,256]{3,2,1,0:T(8,128)(2,1)} %get-tuple-element.79.refs_5_.refs_6_), channel_id=1, source_target_pairs={{0,4},{4,0},{1,5},{5,1},{2,6},{6,2},{3,7},{7,3}} | collective-permute-start | bytes 3145736 | tf_op jit(solution)/shard_map/ppermute | solution.py:617
  262.2 58.0 %collective-permute-start.14 = (bf16[2,2,256,256]{3,2,1,0:T(8,128)(2,1)}, bf16[2,2,256,256]{3,2,1,0:T(8,128)(2,1)}, u32[]{:S(2)}, u32[]{:S(2)}) collective-permute-start(bf16[2,2,256,256]{3,2,1,0:T(8,128)(2,1)} %get-tuple-element.82.refs_6_.refs_7_), channel_id=1, source_target_pairs={{0,4},{4,0},{1,5},{5,1},{2,6},{6,2},{3,7},{7,3}} | collective-permute-start | bytes 1572872 | tf_op jit(solution)/shard_map/ppermute | solution.py:617
  264.0 78.7 %collective-permute-start.15 = (bf16[4,2,256,256]{3,2,1,0:T(8,128)(2,1)}, bf16[4,2,256,256]{3,2,1,0:T(8,128)(2,1)}, u32[]{:S(2)}, u32[]{:S(2)}) collective-permute-start(bf16[4,2,256,256]{3,2,1,0:T(8,128)(2,1)} %get-tuple-element.85.refs_8_.refs_7_), channel_id=1, source_target_pairs={{0,4},{4,0},{1,5},{5,1},{2,6},{6,2},{3,7},{7,3}} | collective-permute-start | bytes 3145736 | tf_op jit(solution)/shard_map/ppermute | solution.py:617
  283.9 68.9 %collective-permute-start.16 = (bf16[2,2,256,256]{3,2,1,0:T(8,128)(2,1)}, bf16[2,2,256,256]{3,2,1,0:T(8,128)(2,1)}, u32[]{:S(2)}, u32[]{:S(2)}) collective-permute-start(bf16[2,2,256,256]{3,2,1,0:T(8,128)(2,1)} %get-tuple-element.88.refs_8_.refs_15_), channel_id=1, source_target_pairs={{0,4},{4,0},{1,5},{5,1},{2,6},{6,2},{3,7},{7,3}} | collective-permute-start | bytes 1572872 | tf_op jit(solution)/shard_map/ppermute | solution.py:617
  286.6 258.6 %collective-permute-start.20 = (bf16[1024,4096]{1,0:T(8,128)(2,1)}, bf16[1024,4096]{1,0:T(8,128)(2,1)}, u32[]{:S(2)}, u32[]{:S(2)}) collective-permute-start(bf16[1024,4096]{1,0:T(8,128)(2,1)} %bitcast.23), channel_id=1, source_target_pairs={{0,1},{1,0},{2,3},{3,2},{4,5},{5,4},{6,7},{7,6}} | collective-permute-start | bytes 25165832 | tf_op jit(solution)/shard_map/ppermute | solution.py:617
  309.0 77.7 %collective-permute-start.24 = (bf16[128,4096]{1,0:T(8,128)(2,1)}, bf16[128,4096]{1,0:T(8,128)(2,1)}, u32[]{:S(2)}, u32[]{:S(2)}) collective-permute-start(bf16[128,4096]{1,0:T(8,128)(2,1)} %get-tuple-element.139), channel_id=1, source_target_pairs={{0,2},{1,3},{2,0},{3,1},{4,6},{5,7},{6,4},{7,5}} | collective-permute-start | bytes 3145736 | tf_op jit(solution)/shard_map/ppermute | solution.py:617
  320.3 98.3 %collective-permute-start.23 = (bf16[128,4096]{1,0:T(8,128)(2,1)}, bf16[128,4096]{1,0:T(8,128)(2,1)}, u32[]{:S(2)}, u32[]{:S(2)}) collective-permute-start(bf16[128,4096]{1,0:T(8,128)(2,1)} %get-tuple-element.140), channel_id=1, source_target_pairs={{0,2},{1,3},{2,0},{3,1},{4,6},{5,7},{6,4},{7,5}} | collective-permute-start | bytes 3145736 | tf_op jit(solution)/shard_map/ppermute | solution.py:617
  342.7 75.9 %collective-permute-start.22 = (bf16[128,4096]{1,0:T(8,128)(2,1)}, bf16[128,4096]{1,0:T(8,128)(2,1)}, u32[]{:S(2)}, u32[]{:S(2)}) collective-permute-start(bf16[128,4096]{1,0:T(8,128)(2,1)} %get-tuple-element.141), channel_id=1, source_target_pairs={{0,2},{1,3},{2,0},{3,1},{4,6},{5,7},{6,4},{7,5}} | collective-permute-start | bytes 3145736 | tf_op jit(solution)/shard_map/ppermute | solution.py:617
  352.8 66.3 %collective-permute-start.25 = (bf16[128,4096]{1,0:T(8,128)(2,1)}, bf16[128,4096]{1,0:T(8,128)(2,1)}, u32[]{:S(2)}, u32[]{:S(2)}) collective-permute-start(bf16[128,4096]{1,0:T(8,128)(2,1)} %collective-permute-done.21.refs_6_), channel_id=1, source_target_pairs={{0,4},{4,0},{1,5},{5,1},{2,6},{6,2},{3,7},{7,3}} | collective-permute-start | bytes 3145736 | tf_op jit(solution)/shard_map/ppermute | solution.py:617
  419.1 48.3 %collective-permute-start.27 = (bf16[128,4096]{1,0:T(8,128)(2,1)}, bf16[128,4096]{1,0:T(8,128)(2,1)}, u32[]{:S(2)}, u32[]{:S(2)}) collective-permute-start(bf16[128,4096]{1,0:T(8,128)(2,1)} %collective-permute-done.23.refs_8_), channel_id=1, source_target_pairs={{0,4},{4,0},{1,5},{5,1},{2,6},{6,2},{3,7},{7,3}} | collective-permute-start | bytes 3145736 | tf_op jit(solution)/shard_map/ppermute | solution.py:617
  420.8 68.6 %collective-permute-start.26 = (bf16[128,4096]{1,0:T(8,128)(2,1)}, bf16[128,4096]{1,0:T(8,128)(2,1)}, u32[]{:S(2)}, u32[]{:S(2)}) collective-permute-start(bf16[128,4096]{1,0:T(8,128)(2,1)} %collective-permute-done.22.refs_7_), channel_id=1, source_target_pairs={{0,4},{4,0},{1,5},{5,1},{2,6},{6,2},{3,7},{7,3}} | collective-permute-start | bytes 3145736 | tf_op jit(solution)/shard_map/ppermute | solution.py:617
  445.9 87.5 %collective-permute-start.32 = (bf16[128,4096]{1,0:T(8,128)(2,1)}, bf16[128,4096]{1,0:T(8,128)(2,1)}, u32[]{:S(2)}, u32[]{:S(2)}) collective-permute-start(bf16[128,4096]{1,0:T(8,128)(2,1)} %collective-permute-done.24.refs_9_), channel_id=1, source_target_pairs={{0,1},{1,0},{2,3},{3,2},{4,5},{5,4},{6,7},{7,6}} | collective-permute-start | bytes 3145736 | tf_op jit(solution)/shard_map/ppermute | solution.py:617
  445.9 87.6 %collective-permute-start.31 = (bf16[128,4096]{1,0:T(8,128)(2,1)}, bf16[128,4096]{1,0:T(8,128)(2,1)}, u32[]{:S(2)}, u32[]{:S(2)}) collective-permute-start(bf16[128,4096]{1,0:T(8,128)(2,1)} %collective-permute-done.23.refs_8_), channel_id=1, source_target_pairs={{0,1},{1,0},{2,3},{3,2},{4,5},{5,4},{6,7},{7,6}} | collective-permute-start | bytes 3145736 | tf_op jit(solution)/shard_map/ppermute | solution.py:617
  467.4 66.6 %collective-permute-start.30 = (bf16[128,4096]{1,0:T(8,128)(2,1)}, bf16[128,4096]{1,0:T(8,128)(2,1)}, u32[]{:S(2)}, u32[]{:S(2)}) collective-permute-start(bf16[128,4096]{1,0:T(8,128)(2,1)} %collective-permute-done.22.refs_7_), channel_id=1, source_target_pairs={{0,1},{1,0},{2,3},{3,2},{4,5},{5,4},{6,7},{7,6}} | collective-permute-start | bytes 3145736 | tf_op jit(solution)/shard_map/ppermute | solution.py:617
  536.0 76.2 %collective-permute-start.38 = (bf16[256,1024]{1,0:T(8,128)(2,1)}, bf16[256,1024]{1,0:T(8,128)(2,1)}, u32[]{:S(2)}, u32[]{:S(2)}) collective-permute-start(bf16[256,1024]{1,0:T(8,128)(2,1)} %get-tuple-element.105), channel_id=1, source_target_pairs={{0,1},{1,0},{2,3},{3,2},{4,5},{5,4},{6,7},{7,6}} | collective-permute-start | bytes 1572872 | tf_op jit(solution)/shard_map/ppermute | solution.py:617
  537.5 74.7 %collective-permute-start.39 = (bf16[256,1024]{1,0:T(8,128)(2,1)}, bf16[256,1024]{1,0:T(8,128)(2,1)}, u32[]{:S(2)}, u32[]{:S(2)}) collective-permute-start(bf16[256,1024]{1,0:T(8,128)(2,1)} %get-tuple-element.106), channel_id=1, source_target_pairs={{0,2},{1,3},{2,0},{3,1},{4,6},{5,7},{6,4},{7,5}} | collective-permute-start | bytes 1572872 | tf_op jit(solution)/shard_map/ppermute | solution.py:617
  543.6 68.6 %collective-permute-start.40 = (bf16[256,1024]{1,0:T(8,128)(2,1)}, bf16[256,1024]{1,0:T(8,128)(2,1)}, u32[]{:S(2)}, u32[]{:S(2)}) collective-permute-start(bf16[256,1024]{1,0:T(8,128)(2,1)} %get-tuple-element.107), channel_id=1, source_target_pairs={{0,3},{1,2},{2,1},{3,0},{4,7},{5,6},{6,5},{7,4}} | collective-permute-start | bytes 1572872 | tf_op jit(solution)/shard_map/ppermute | solution.py:617
  565.0 67.3 %collective-permute-start.37 = (bf16[256,4096]{1,0:T(8,128)(2,1)}, bf16[256,4096]{1,0:T(8,128)(2,1)}, u32[]{:S(2)}, u32[]{:S(2)}) collective-permute-start(bf16[256,4096]{1,0:T(8,128)(2,1)} %get-tuple-element.104.refs_0_), channel_id=1, source_target_pairs={{0,2},{1,3},{2,0},{3,1},{4,6},{5,7},{6,4},{7,5}} | collective-permute-start | bytes 6291464 | tf_op jit(solution)/shard_map/ppermute | solution.py:617
  566.5 66.2 %collective-permute-start.41 = (bf16[256,4096]{1,0:T(8,128)(2,1)}, bf16[256,4096]{1,0:T(8,128)(2,1)}, u32[]{:S(2)}, u32[]{:S(2)}) collective-permute-start(bf16[256,4096]{1,0:T(8,128)(2,1)} %get-tuple-element.104.refs_0_), channel_id=1, source_target_pairs={{0,1},{1,0},{2,3},{3,2},{4,5},{5,4},{6,7},{7,6}} | collective-permute-start | bytes 6291464 | tf_op jit(solution)/shard_map/ppermute | solution.py:617
  726.9 90.0 %collective-permute-start.43 = (bf16[512,4096]{1,0:T(8,128)(2,1)}, bf16[512,4096]{1,0:T(8,128)(2,1)}, u32[]{:S(2)}, u32[]{:S(2)}) collective-permute-start(bf16[512,4096]{1,0:T(8,128)(2,1)} %get-tuple-element.114), channel_id=1, source_target_pairs={{0,1},{1,0},{2,3},{3,2},{4,5},{5,4},{6,7},{7,6}} | collective-permute-start | bytes 12582920 | tf_op jit(solution)/shard_map/ppermute | solution.py:617
  727.3 48.8 %collective-permute-start.49 = (bf16[256,4096]{1,0:T(8,128)(2,1)}, bf16[256,4096]{1,0:T(8,128)(2,1)}, u32[]{:S(2)}, u32[]{:S(2)}) collective-permute-start(bf16[256,4096]{1,0:T(8,128)(2,1)} %get-tuple-element.121.refs_0_), channel_id=1, source_target_pairs={{0,2},{1,3},{2,0},{3,1},{4,6},{5,7},{6,4},{7,5}} | collective-permute-start | bytes 6291464 | tf_op jit(solution)/shard_map/ppermute | solution.py:617
  727.3 48.8 %collective-permute-start.44 = (bf16[256,1024]{1,0:T(8,128)(2,1)}, bf16[256,1024]{1,0:T(8,128)(2,1)}, u32[]{:S(2)}, u32[]{:S(2)}) collective-permute-start(bf16[256,1024]{1,0:T(8,128)(2,1)} %get-tuple-element.115), channel_id=1, source_target_pairs={{0,1},{1,0},{2,3},{3,2},{4,5},{5,4},{6,7},{7,6}} | collective-permute-start | bytes 1572872 | tf_op jit(solution)/shard_map/ppermute | solution.py:617
  727.4 59.9 %collective-permute-start.45 = (bf16[256,1024]{1,0:T(8,128)(2,1)}, bf16[256,1024]{1,0:T(8,128)(2,1)}, u32[]{:S(2)}, u32[]{:S(2)}) collective-permute-start(bf16[256,1024]{1,0:T(8,128)(2,1)} %get-tuple-element.116), channel_id=1, source_target_pairs={{0,2},{1,3},{2,0},{3,1},{4,6},{5,7},{6,4},{7,5}} | collective-permute-start | bytes 1572872 | tf_op jit(solution)/shard_map/ppermute | solution.py:617
  729.3 67.6 %collective-permute-start.46 = (bf16[256,1024]{1,0:T(8,128)(2,1)}, bf16[256,1024]{1,0:T(8,128)(2,1)}, u32[]{:S(2)}, u32[]{:S(2)}) collective-permute-start(bf16[256,1024]{1,0:T(8,128)(2,1)} %get-tuple-element.117), channel_id=1, source_target_pairs={{0,3},{1,2},{2,1},{3,0},{4,7},{5,6},{6,5},{7,4}} | collective-permute-start | bytes 1572872 | tf_op jit(solution)/shard_map/ppermute | solution.py:617
  776.1 45.1 %collective-permute-start.50 = (bf16[256,4096]{1,0:T(8,128)(2,1)}, bf16[256,4096]{1,0:T(8,128)(2,1)}, u32[]{:S(2)}, u32[]{:S(2)}) collective-permute-start(bf16[256,4096]{1,0:T(8,128)(2,1)} %get-tuple-element.121.refs_0_), channel_id=1, source_target_pairs={{0,1},{1,0},{2,3},{3,2},{4,5},{5,4},{6,7},{7,6}} | collective-permute-start | bytes 6291464 | tf_op jit(solution)/shard_map/ppermute | solution.py:617
  776.1 45.1 %collective-permute-start.51 = (bf16[256,4096]{1,0:T(8,128)(2,1)}, bf16[256,4096]{1,0:T(8,128)(2,1)}, u32[]{:S(2)}, u32[]{:S(2)}) collective-permute-start(bf16[256,4096]{1,0:T(8,128)(2,1)} %collective-permute-done.49.refs_1_), channel_id=1, source_target_pairs={{0,1},{1,0},{2,3},{3,2},{4,5},{5,4},{6,7},{7,6}} | collective-permute-start | bytes 6291464 | tf_op jit(solution)/shard_map/ppermute | solution.py:617
  911.4 90.0 %collective-permute-start.57 = (bf16[512,4096]{1,0:T(8,128)(2,1)}, bf16[512,4096]{1,0:T(8,128)(2,1)}, u32[]{:S(2)}, u32[]{:S(2)}) collective-permute-start(bf16[512,4096]{1,0:T(8,128)(2,1)} %get-tuple-element.130), channel_id=1, source_target_pairs={{0,1},{1,0},{2,3},{3,2},{4,5},{5,4},{6,7},{7,6}} | collective-permute-start | bytes 12582920 | tf_op jit(solution)/shard_map/ppermute | solution.py:617
  912.1 48.8 %collective-permute-start.48 = (bf16[256,4096]{1,0:T(8,128)(2,1)}, bf16[256,4096]{1,0:T(8,128)(2,1)}, u32[]{:S(2)}, u32[]{:S(2)}) collective-permute-start(bf16[256,4096]{1,0:T(8,128)(2,1)} %get-tuple-element.120.refs_0_), channel_id=1, source_target_pairs={{0,2},{1,3},{2,0},{3,1},{4,6},{5,7},{6,4},{7,5}} | collective-permute-start | bytes 6291464 | tf_op jit(solution)/shard_map/ppermute | solution.py:617
  912.3 48.6 %collective-permute-start.54 = (bf16[256,1024]{1,0:T(8,128)(2,1)}, bf16[256,1024]{1,0:T(8,128)(2,1)}, u32[]{:S(2)}, u32[]{:S(2)}) collective-permute-start(bf16[256,1024]{1,0:T(8,128)(2,1)} %get-tuple-element.125), channel_id=1, source_target_pairs={{0,1},{1,0},{2,3},{3,2},{4,5},{5,4},{6,7},{7,6}} | collective-permute-start | bytes 1572872 | tf_op jit(solution)/shard_map/ppermute | solution.py:617
  912.3 59.8 %collective-permute-start.55 = (bf16[256,1024]{1,0:T(8,128)(2,1)}, bf16[256,1024]{1,0:T(8,128)(2,1)}, u32[]{:S(2)}, u32[]{:S(2)}) collective-permute-start(bf16[256,1024]{1,0:T(8,128)(2,1)} %get-tuple-element.126), channel_id=1, source_target_pairs={{0,2},{1,3},{2,0},{3,1},{4,6},{5,7},{6,4},{7,5}} | collective-permute-start | bytes 1572872 | tf_op jit(solution)/shard_map/ppermute | solution.py:617
  914.1 67.4 %collective-permute-start.56 = (bf16[256,1024]{1,0:T(8,128)(2,1)}, bf16[256,1024]{1,0:T(8,128)(2,1)}, u32[]{:S(2)}, u32[]{:S(2)}) collective-permute-start(bf16[256,1024]{1,0:T(8,128)(2,1)} %get-tuple-element.127), channel_id=1, source_target_pairs={{0,3},{1,2},{2,1},{3,0},{4,7},{5,6},{6,5},{7,4}} | collective-permute-start | bytes 1572872 | tf_op jit(solution)/shard_map/ppermute | solution.py:617
  960.9 44.8 %collective-permute-start.52 = (bf16[256,4096]{1,0:T(8,128)(2,1)}, bf16[256,4096]{1,0:T(8,128)(2,1)}, u32[]{:S(2)}, u32[]{:S(2)}) collective-permute-start(bf16[256,4096]{1,0:T(8,128)(2,1)} %get-tuple-element.120.refs_0_), channel_id=1, source_target_pairs={{0,1},{1,0},{2,3},{3,2},{4,5},{5,4},{6,7},{7,6}} | collective-permute-start | bytes 6291464 | tf_op jit(solution)/shard_map/ppermute | solution.py:617
  1096.0 99.2 %collective-permute-start.62 = (bf16[512,4096]{1,0:T(8,128)(2,1)}, bf16[512,4096]{1,0:T(8,128)(2,1)}, u32[]{:S(2)}, u32[]{:S(2)}) collective-permute-start(bf16[512,4096]{1,0:T(8,128)(2,1)} %get-tuple-element.135), channel_id=1, source_target_pairs={{0,1},{1,0},{2,3},{3,2},{4,5},{5,4},{6,7},{7,6}} | collective-permute-start | bytes 12582920 | tf_op jit(solution)/shard_map/ppermute | solution.py:617
  1096.8 48.8 %collective-permute-start.59 = (bf16[256,4096]{1,0:T(8,128)(2,1)}, bf16[256,4096]{1,0:T(8,128)(2,1)}, u32[]{:S(2)}, u32[]{:S(2)}) collective-permute-start(bf16[256,4096]{1,0:T(8,128)(2,1)} %get-tuple-element.132.refs_0_), channel_id=1, source_target_pairs={{0,2},{1,3},{2,0},{3,1},{4,6},{5,7},{6,4},{7,5}} | collective-permute-start | bytes 6291464 | tf_op jit(solution)/shard_map/ppermute | solution.py:617
  1097.2 92.5 %collective-permute-start.47 = (bf16[256,4096]{1,0:T(8,128)(2,1)}, bf16[256,4096]{1,0:T(8,128)(2,1)}, u32[]{:S(2)}, u32[]{:S(2)}) collective-permute-start(bf16[256,4096]{1,0:T(8,128)(2,1)} %add_convert_fusion.3.refs_7_), channel_id=1, source_target_pairs={{0,2},{1,3},{2,0},{3,1},{4,6},{5,7},{6,4},{7,5}} | collective-permute-start | bytes 6291464 | tf_op jit(solution)/shard_map/ppermute | solution.py:617
  1098.8 100.8 %collective-permute-start.60 = (bf16[256,4096]{1,0:T(8,128)(2,1)}, bf16[256,4096]{1,0:T(8,128)(2,1)}, u32[]{:S(2)}, u32[]{:S(2)}) collective-permute-start(bf16[256,4096]{1,0:T(8,128)(2,1)} %get-tuple-element.132.refs_0_), channel_id=1, source_target_pairs={{0,1},{1,0},{2,3},{3,2},{4,5},{5,4},{6,7},{7,6}} | collective-permute-start | bytes 6291464 | tf_op jit(solution)/shard_map/ppermute | solution.py:617
  1145.6 54.0 %collective-permute-start.61 = (bf16[256,4096]{1,0:T(8,128)(2,1)}, bf16[256,4096]{1,0:T(8,128)(2,1)}, u32[]{:S(2)}, u32[]{:S(2)}) collective-permute-start(bf16[256,4096]{1,0:T(8,128)(2,1)} %collective-permute-done.59.refs_1_), channel_id=1, source_target_pairs={{0,1},{1,0},{2,3},{3,2},{4,5},{5,4},{6,7},{7,6}} | collective-permute-start | bytes 6291464 | tf_op jit(solution)/shard_map/ppermute | solution.py:617
  1289.6 54.4 %collective-permute-start.64 = (bf16[512,4096]{1,0:T(8,128)(2,1)}, bf16[512,4096]{1,0:T(8,128)(2,1)}, u32[]{:S(2)}, u32[]{:S(2)}) collective-permute-start(bf16[512,4096]{1,0:T(8,128)(2,1)} %get-tuple-element.138), channel_id=1, source_target_pairs={{0,1},{1,0},{2,3},{3,2},{4,5},{5,4},{6,7},{7,6}} | collective-permute-start | bytes 12582920 | tf_op jit(solution)/shard_map/ppermute | solution.py:617
  1289.7 48.8 %collective-permute-start.58 = (bf16[256,4096]{1,0:T(8,128)(2,1)}, bf16[256,4096]{1,0:T(8,128)(2,1)}, u32[]{:S(2)}, u32[]{:S(2)}) collective-permute-start(bf16[256,4096]{1,0:T(8,128)(2,1)} %add_convert_fusion.2.refs_7_), channel_id=1, source_target_pairs={{0,2},{1,3},{2,0},{3,1},{4,6},{5,7},{6,4},{7,5}} | collective-permute-start | bytes 6291464 | tf_op jit(solution)/shard_map/ppermute | solution.py:617
  1290.0 93.4 %collective-permute-start.63 = (bf16[256,4096]{1,0:T(8,128)(2,1)}, bf16[256,4096]{1,0:T(8,128)(2,1)}, u32[]{:S(2)}, u32[]{:S(2)}) collective-permute-start(bf16[256,4096]{1,0:T(8,128)(2,1)} %add_convert_fusion.1.refs_7_), channel_id=1, source_target_pairs={{0,2},{1,3},{2,0},{3,1},{4,6},{5,7},{6,4},{7,5}} | collective-permute-start | bytes 6291464 | tf_op jit(solution)/shard_map/ppermute | solution.py:617
  1348.4 79.5 %collective-permute-start.65 = (bf16[256,4096]{1,0:T(8,128)(2,1)}, bf16[256,4096]{1,0:T(8,128)(2,1)}, u32[]{:S(2)}, u32[]{:S(2)}) collective-permute-start(bf16[256,4096]{1,0:T(8,128)(2,1)} %add_convert_fusion.refs_5_), channel_id=1, source_target_pairs={{0,2},{1,3},{2,0},{3,1},{4,6},{5,7},{6,4},{7,5}} | collective-permute-start | bytes 6291464 | tf_op jit(solution)/shard_map/ppermute | solution.py:617
  (20 other events, 359.1 us)

commit v5 on v4

--- a/solution.py
+++ b/solution.py
@@ -42,14 +42,6 @@
 def ordered(kernel, n_in, after):
     n = len(after)
     return lambda *refs: kernel(*refs[:n_in], *refs[n_in + n:])
-
-
-def load_all(pairs, sem):
-    copies = [pltpu.make_async_copy(src, dst, sem.at[i]) for i, (src, dst) in enumerate(pairs)]
-    for cp in copies:
-        cp.start()
-    for cp in copies:
-        cp.wait()
 
 
 def norm_kernel(x_ref, g_ref, o_ref):
@@ -140,7 +132,7 @@
 
 
 BLK = 12
-MASK0, MASK1, LAST, FIRST, CARRY = 1, 2, 4, 8, 16
+LAST, FIRST, CARRY = 16, 32, 64
 ST = HD + 16
 
 
@@ -182,40 +174,51 @@
         lax.fori_loop(have, need, one, 0)
         return jnp.maximum(have, need)
 
-    def put(s, slot):
-        s_scr[slot] = s
-        mb = jnp.max(s.reshape(2 * RUN // 8, 8, T), axis=0)
+    def put(s, h, k):
+        s_scr[h, pl.ds(k * RUN, RUN), :] = s
+        mb_scr[h, k] = jnp.max(s.reshape(RUN // 8, 8, T), axis=0)
+
+    def stage_a(row, g, h):
+        col = pl.multiple_of(g * HD, HD)
+        qt = q_scr[tab_ref[row], pl.ds(pl.multiple_of((g * G + h) * HD, HD), HD), :]
+        for k in range(4):
+            put(lax.dot_general(kv_scr[tab_ref[row + 3 + k], 0, :, pl.ds(col, HD)], qt, DN, preferred_element_type=F32), h, k)
+
+    def stage_b(row, g, h):
+        col = pl.multiple_of(g * HD, HD)
+        m_prev = m_scr[h]
+        mb = jnp.maximum(jnp.maximum(mb_scr[h, 0], mb_scr[h, 1]), jnp.maximum(mb_scr[h, 2], mb_scr[h, 3]))
         for r in (4, 2, 1):
             mb = jnp.maximum(mb, pltpu.roll(mb, r, 0))
-        mb_scr[slot] = mb
-
-    def stage_a(row, g, it, h):
-        col = pl.multiple_of(g * HD, HD)
-        qt = q_scr[tab_ref[row], pl.ds(pl.multiple_of((g * G + h) * HD, HD), HD), :]
-        put(jnp.concatenate([lax.dot_general(kv_scr[tab_ref[row + 3 + 2 * it + k], 0, :, pl.ds(col, HD)], qt, DN,
-                                             preferred_element_type=F32) for k in range(2)], axis=0), it * G + h)
-
-    def stage_b(row, g, it, h):
-        slot = it * G + h
-        col = pl.multiple_of(g * HD, HD)
-        m_prev = m_scr[h]
-        m_new = jnp.maximum(m_prev, mb_scr[slot])
+        m_new = jnp.maximum(m_prev, mb)
         m_scr[h] = m_new
         m_c = m_new * c
-        p = jnp.exp2(s_scr[slot].reshape(2 * RUN // 8, 8, T) * c - m_c[None])
         alpha = jnp.exp2(m_prev * c - m_c)
-        l_scr[h] = l_scr[h] * alpha + jnp.sum(p, axis=0)
-        pb = p.reshape(2 * RUN, T).astype(BF)
-        pv = sum(lax.dot_general(kv_scr[tab_ref[row + 3 + 2 * it + k], 1, pl.ds(col, HD), :], pb[k * RUN:(k + 1) * RUN], DN,
-                                 preferred_element_type=F32) for k in range(2))
+        l, pv = l_scr[h] * alpha, None
+        for k in range(4):
+            p = jnp.exp2(s_scr[h, k * RUN:(k + 1) * RUN].reshape(RUN // 8, 8, T) * c - m_c[None])
+            l = l + jnp.sum(p, axis=0)
+            d = lax.dot_general(kv_scr[tab_ref[row + 3 + k], 1, pl.ds(col, HD), :], p.reshape(RUN, T).astype(BF), DN,
+                                preferred_element_type=F32)
+            pv = d if pv is None else pv + d
+        l_scr[h] = l
         acc_scr[h] = (acc_scr[h].reshape(HD // 8, 8, T) * alpha[None]).reshape(HD, T) + pv
 
-    def mask_item(row, it):
+    def mask_runs(row, flags):
+        qry = lax.broadcasted_iota(jnp.int32, (RUN, T), 1) + tab_ref[base + 1 + tab_ref[row]]
         key = lax.broadcasted_iota(jnp.int32, (RUN, T), 0)
-        qry = lax.broadcasted_iota(jnp.int32, (RUN, T), 1) + tab_ref[base + 1 + tab_ref[row]]
-        mask = jnp.concatenate([key + tab_ref[row + 7 + 2 * it + k] <= qry for k in range(2)], axis=0)
-        for h in range(G):
-            put(jnp.where(mask, s_scr[it * G + h], NEG), it * G + h)
+
+        def one(k, carry):
+            @pl.when((lax.shift_right_logical(flags, k) & 1) != 0)
+            def _():
+                mask = key + tab_ref[row + 7 + k] <= qry
+                rows = pl.multiple_of(k * RUN, RUN)
+                for h in range(G):
+                    put(jnp.where(mask, s_scr[h, pl.ds(rows, RUN), :], NEG), h, k)
+
+            return carry
+
+        lax.fori_loop(0, 4, one, 0)
 
     def finish(tile, g, get):
         for h in range(G):
@@ -247,9 +250,8 @@
 
     row, g = block(0)
     have = arrived(0, tab_ref[row + 2])
-    for it in range(2):
-        for h in range(G):
-            stage_a(row, g, it, h)
+    for h in range(G):
+        stage_a(row, g, h)
 
     def body(i, have):
         row, g = block(i)
@@ -276,18 +278,13 @@
                     m_scr[h] = st_scr[tile, g, h, HD:HD + 8, :]
                     l_scr[h] = st_scr[tile, g, h, HD + 8:, :]
 
-        @pl.when((flags & MASK0) != 0)
+        @pl.when((flags & 15) != 0)
         def _():
-            mask_item(row, 0)
-
-        @pl.when((flags & MASK1) != 0)
-        def _():
-            mask_item(row, 1)
-
-        for it in range(2):
-            for h in range(G):
-                stage_b(row, g, it, h)
-                stage_a(nrow, ng, it, h)
+            mask_runs(row, flags)
+
+        for h in range(G):
+            stage_b(row, g, h)
+            stage_a(nrow, ng, h)
 
         @pl.when((flags & LAST) != 0)
         def _():
@@ -332,7 +329,6 @@
     final = st_tiles is None
     kv_src = [(a, i) for a, kv in enumerate(kvs) for i in range(kv.shape[0])]
     n_runs = len(kv_src)
-    slots = 2 * G
     sts = () if st is None else (st,)
     n_in = 1 + len(qs) + len(kvs) + len(sts)
     state = (n_heads, G, ST, RUN)
@@ -349,8 +345,8 @@
                             pltpu.VMEM((n_runs, 2, 256, 256), BF),
                             pltpu.VMEM((n_tiles if final else 1, RUN, nq), BF),
                             pltpu.VMEM((n_tiles if has_st else 1, *state), F32),
-                            pltpu.VMEM((slots, 2 * RUN, RUN), F32),
-                            pltpu.VMEM((slots, 8, RUN), F32),
+                            pltpu.VMEM((G, 4 * RUN, RUN), F32),
+                            pltpu.VMEM((G, 4, 8, RUN), F32),
                             pltpu.VMEM((G, HD, RUN), F32),
                             pltpu.VMEM((G, 8, RUN), F32),
                             pltpu.VMEM((G, 8, RUN), F32),
@@ -367,9 +363,11 @@
     )(tab, *qs, *kvs, *sts, *after)
 
 
-def out_kernel(*refs, blocks, n_w):
-    o_refs, w_refs = refs[:4], refs[4:4 + n_w]
-    x_ref, g_ref, y_ref, b_ref, o_scr, w_scr, acc_scr, o_sem, w_sem = refs[4 + n_w:]
+def out_kernel(*refs, blocks, n_w, n_run):
+    n_o = 4 * n_run
+    o_refs, w_refs, x_ref, g_ref = refs[:n_o], refs[n_o:n_o + n_w], refs[n_o + n_w], refs[n_o + n_w + 1]
+    outs = refs[n_o + n_w + 2:n_o + n_w + 2 + 2 * n_run]
+    o_scr, w_scr, acc_scr, o_sem, w_sem = refs[n_o + n_w + 2 + 2 * n_run:]
     width = o_refs[0].shape[1]
     half = width // 2
     n_slots = w_scr.shape[0]
@@ -384,16 +382,23 @@
                                           w_sem.at[i % n_slots]).start()
                     at += n
 
+    mine = lax.axis_index('cp')
+    pairs = []
+    for i in range(n_run):
+        os, rows = o_refs[4 * i:4 * i + 4], pl.ds(i * RUN, RUN)
+        pairs += [(os[0], o_scr.at[rows, pl.ds(0, width)]), (os[1], o_scr.at[rows, pl.ds(width, width)])]
+        for k in range(2, 4):
+            for p, part in enumerate((mine, 1 - mine)):
+                pairs.append((os[k].at[:, pl.ds(pl.multiple_of(part * half, half), half)],
+                              o_scr.at[rows, pl.ds(k * width + p * half, half)]))
+    copies = [pltpu.make_async_copy(src, dst, o_sem.at[i]) for i, (src, dst) in enumerate(pairs)]
+    for cp in copies:
+        cp.start()
     for i in range(n_slots - 1):
         fetch(jnp.int32(i))
-    mine = lax.axis_index('cp')
-    pairs = [(o_refs[0], o_scr.at[:, pl.ds(0, width)]), (o_refs[1], o_scr.at[:, pl.ds(width, width)])]
-    for k in range(2, 4):
-        for p, part in enumerate((mine, 1 - mine)):
-            pairs.append((o_refs[k].at[:, pl.ds(pl.multiple_of(part * half, half), half)],
-                          o_scr.at[:, pl.ds(k * width + p * half, half)]))
-    load_all(pairs, o_sem)
     acc_scr[...] = jnp.zeros_like(acc_scr)
+    for cp in copies:
+        cp.wait()
 
     def one(k, carry):
         fetch(k + n_slots - 1)
@@ -404,32 +409,35 @@
 
     lax.fori_loop(0, len(blocks), one, 0)
 
-    def rows32(i, carry):
-        rows = pl.ds(pl.multiple_of(i * 32, 32), 32)
-        y = (x_ref[rows, :].astype(F32) + acc_scr[rows, :].astype(BF).astype(F32)).astype(BF)
-        y_ref[rows, :] = y
-        b_ref[rows, :] = norm_rows(y, g_ref[...])
-        return carry
-
-    lax.fori_loop(0, RUN // 32, rows32, 0)
-
-
-def out_proj(os, ws, blocks, x_rows, gain, j, after=()):
+    for i in range(n_run):
+        def rows32(r, carry):
+            at = pl.multiple_of(r * 32, 32)
+            rows, mine = pl.ds(at, 32), pl.ds(i * RUN + at, 32)
+            y = (x_ref[mine, :].astype(F32) + acc_scr[mine, :].astype(BF).astype(F32)).astype(BF)
+            outs[2 * i][rows, :] = y
+            outs[2 * i + 1][rows, :] = norm_rows(y, g_ref[...])
+            return carry
+
+        lax.fori_loop(0, RUN // 32, rows32, 0)
+
+
+def out_proj(os, ws, blocks, x_rows, gain, at, after=()):
     dim = x_rows.shape[1]
     width = os[0].shape[1]
-    one = lambda s: pl.BlockSpec((RUN, dim), lambda i: (s, 0))
-    n_after = len(after)
+    n_run = len(os) // 4
+    rows = n_run * RUN
+    one = lambda m, s: pl.BlockSpec((m, dim), lambda i: (s, 0))
     return pl.pallas_call(
-        ordered(functools.partial(out_kernel, blocks=blocks, n_w=len(ws)), 6 + len(ws), after),
+        ordered(functools.partial(out_kernel, blocks=blocks, n_w=len(ws), n_run=n_run), len(os) + len(ws) + 2, after),
         grid=(1,),
-        in_specs=[ANY] * (4 + len(ws)) + [one(j), pl.BlockSpec((1, dim), lambda i: (0, 0))] + [ANY] * n_after,
-        out_specs=[one(0)] * 2,
-        out_shape=[jax.ShapeDtypeStruct((RUN, dim), BF)] * 2,
-        scratch_shapes=[pltpu.VMEM((RUN, 4 * width), BF), pltpu.VMEM((3, width // 2, dim), BF), pltpu.VMEM((RUN, dim), F32),
-                        pltpu.SemaphoreType.DMA((6,)), pltpu.SemaphoreType.DMA((3,))],
+        in_specs=[ANY] * (len(os) + len(ws)) + [one(rows, at), pl.BlockSpec((1, dim), lambda i: (0, 0))] + [ANY] * len(after),
+        out_specs=[one(RUN, 0)] * (2 * n_run),
+        out_shape=[jax.ShapeDtypeStruct((RUN, dim), BF)] * (2 * n_run),
+        scratch_shapes=[pltpu.VMEM((rows, 4 * width), BF), pltpu.VMEM((3, width // 2, dim), BF), pltpu.VMEM((rows, dim), F32),
+                        pltpu.SemaphoreType.DMA((6 * n_run,)), pltpu.SemaphoreType.DMA((3,))],
         name="outp", compiler_params=params(1),
-        cost_estimate=pl.CostEstimate(flops=8 * RUN * width * dim, transcendentals=0,
-                                      bytes_accessed=8 * width * dim + 8 * RUN * dim),
+        cost_estimate=pl.CostEstimate(flops=8 * rows * width * dim, transcendentals=0,
+                                      bytes_accessed=8 * width * dim + 8 * rows * dim),
     )(*os, *ws, x_rows, gain, *after)
 
 
@@ -536,7 +544,7 @@
     blocks = [[0, runs[i:i + 4]] for i in range(0, len(runs), 4)]
     if tail:
         full = tail + [(tail[0][0], FAR)] * (4 - len(tail))
-        flags = (MASK0 if diag is not None or len(tail) < 2 else 0) | (MASK1 if len(tail) < 4 else 0)
+        flags = sum(1 << k for k, (r, p) in enumerate(full) if p == FAR or r == diag)
         blocks.append([flags, full])
     blocks[-1][0] |= LAST
     blocks[0][0] |= FIRST
@@ -561,10 +569,9 @@
 def work_tables(cps, piece):
     per = piece // 2 // RUN
     early = 2 * per + 2
-    later = early + 4
-    stage = lambda r: 0 if r < early else 1 if r < later else 2
-    calls = [(0, list(range(early))), (1, list(range(later)))]
-    calls += [(2, [j, per + j, 2 * per + 2 * j, 2 * per + 2 * j + 1]) for j in range(per)]
+    stage = lambda r: 0 if r < early else 1
+    calls = [(0, list(range(early)))]
+    calls += [(1, [j, per + j, 2 * per + 2 * j, 2 * per + 2 * j + 1]) for j in range(per)]
     tabs, all_runs, sizes = [], [], []
     for y in range(cps):
         for xi in range(2):
@@ -580,7 +587,7 @@
                         seen = [r for r in range(len(pos)) if pos[r] < pos[t]]
                         pairs.append(([r for r in seen if max(stage(r), stage(t)) == now], stage(t) == now))
                         carry.append(int(stage(t) < now))
-                    tab, n = call_table(tiles, pos, pairs, carry, 2 if now == 2 else 0)
+                    tab, n = call_table(tiles, pos, pairs, carry, 2 if now == 1 else 0)
                     tabs[-1].append(tab)
                     sizes[-1].append(n)
     widths = [max(len(t[k]) for t in tabs) for k in range(len(calls))]
@@ -647,12 +654,9 @@
         tile = lambda a, n: [(a, i) for i in range(n)]
         tiles = tile(0, n_run) + tile(1, n_run) + tile(2, 2)
         st, = flash(tab, [q_own, q_mate, q_a], tiles, [kv_own, kv_mate, kv_a], base=bases[0],
-                   work=int(work[0]), st_tiles=len(tiles) + 4)
+                   work=int(work[0]), st_tiles=len(tiles))
         q_b, kv_b = qkv(early + relayed(2, st), w_all, (tables, 2 * n_run), after=(st,))
-        st, = flash(tab, [q_own, q_mate, q_a, q_b], tiles + tile(3, 4), [kv_own, kv_mate, kv_a, kv_b],
-                   base=bases[1], work=int(work[1]), st=st, st_src=list(range(len(tiles))) + [None] * 4,
-                   st_tiles=len(tiles) + 4)
-        q_c, kv_c = qkv(relayed(3, st), w_all, (tables, 2 * n_run + 6), after=(st,))
+        q_c, kv_c = qkv(relayed(3, kv_b), w_all, (tables, 2 * n_run + 6), after=(kv_b,))
         kvs = [kv_own, kv_mate, kv_a, kv_b, kv_c]
         kvs = kvs + [send(over_y, kv) for kv in kvs]
         q_far = [(q_a, 0), (q_b, 0), (q_b, 2), (q_c, 0)]
@@ -672,23 +676,25 @@
         def attend(j):
             q, at = q_far[j]
             held = 2 * n_run + 2 * j
-            carried = [j, n_run + j] + ([held, held + 1] if j + 1 < n_run else [None, None])
+            carried = [j, n_run + j] + ([held, held + 1] if j == 0 else [None, None])
             o_own, o_mate, o_far, o_fm = flash(
                 tab, [q_own, q_mate, q], [(0, j), (1, j), (2, at), (2, at + 1)], kvs,
-                base=bases[2 + j], work=int(work[2 + j]), st=st, st_src=carried, after=(prev,))
+                base=bases[1 + j], work=int(work[1 + j]), st=st, st_src=carried, after=(prev,))
             os.append([o_own, send(over_core, o_mate), send(over_x, o_far), send(over_both, o_fm)])
             return o_own
 
-        def project(j):
+        def project(i):
             ws = [wo, wo_c]
             blocks = [[(0, 0, half)], [(0, half, half)], [(1, 0, half)], [(1, half, half)]]
             for k in range(2):
                 for held in (wo_ya, wo_yb):
                     blocks.append([(len(ws) + p, 0, rows) for p in range(n_piece)])
                     ws += [held[p][k] for p in range(n_piece)]
-            y, b = out_proj(os[j], ws, blocks, x_rows, gm, j, after=(prev,))
-            outs.append((y, b, send(over_x, b), send(over_core, b)))
-            return y
+            got = out_proj(os[2 * i] + os[2 * i + 1], ws, blocks, x_rows, gm, i, after=(prev,))
+            for k in range(2):
+                y, b = got[2 * k:2 * k + 2]
+                outs.append((y, b, send(over_x, b), send(over_core, b)))
+            return got[0]
 
         forward_w(0)
         prev = attend(0)
@@ -703,7 +709,6 @@
         relay_w(3)
         prev = project(0)
         prev = attend(3)
-        prev = project(1)
 
         z, sums, relay = None, [], {}
 
@@ -722,11 +727,11 @@
             prev = keep
             if j + 1 < n_run:
                 relay_b(j + 1)
-            if j + 2 < n_run:
-                prev = project(j + 2)
-            else:
+            if j == 0:
+                prev = project(1)
+            elif j > 1:
                 prev = z = finish(j - 2)
-            kept = tied(keep, prev)
+            kept = keep if prev is keep else tied(keep, prev)
             prev = s_far = (kept[RUN:].astype(F32) + recv[RUN:].astype(F32)).astype(BF)
             sums.append((keep, recv, send(over_x, s_far), y))
         for j in range(n_run - 2, n_run):

time: 1440 us -> 1390 us (0.965)
  Pallas kernels: 820 us -> 773 us
    pallas_call x6 -> x5, Pallas kernels: 247 us -> 216 us  [flash(): pl.pallas_call(ordered(functools.partial(flash_kernel, q_src=q_src, kv_sr...]
    pallas_call x4 -> x2, Pallas kernels: 79.7 us -> 63.1 us  [out_proj(): pl.pallas_call(ordered(functools.partial(out_kernel, blocks=blocks, n_w=l...]
  transfers between devices with their start and end apart: 66 -> 66, of which waited for: 26 -> 30; matrix products, arithmetic and copies ran while one was open for 3% -> 3% of each run, Pallas kernels for 31% -> 34%
where the time goes in v5:
time: 1390 us; the launch traced here: 1380 us
  Pallas kernels  773 us (56%)
  waiting for transfers between devices  502 us (36%)
  starting transfers between devices  54.9 us (4%)
  local copies, waits for them, and re-layouts  23.6 us (2%)
  other arithmetic  23.1 us (2%)
    ppermute x66, waiting for transfers between devices, send(): return lax.ppermute(v, *axis_pairs)  502 us
    pallas_call x4, Pallas kernels, mlp(): pl.pallas_call(ordered(functools.partial(mlp_kernel, n_in=len(bs), tn=tn,...  361 us
    pallas_call x5, Pallas kernels, flash(): pl.pallas_call(ordered(functools.partial(flash_kernel, q_src=q_src, kv_sr...  216 us
    pallas_call x5, Pallas kernels, qkv(): pl.pallas_call(ordered(functools.partial(qkv_kernel, n_in=n_in, n_q=n_q,...  96.5 us
    pallas_call x2, Pallas kernels, out_proj(): pl.pallas_call(ordered(functools.partial(out_kernel, blocks=blocks, n_w=l...  63.1 us
    ppermute x66, starting transfers between devices, send(): return lax.ppermute(v, *axis_pairs)  54.9 us
  transfers between devices with their start and end apart: 66, of which 30 were waited for; matrix products, arithmetic and copies ran while one was open for 3% of the time, Pallas kernels for 34%

profile of v5, /device:TPU:0, one launch (start us, length us, event | category | flops | bytes accessed | tf_op | source)
XLA Modules:
  0.0 1377.1 jit_solution(4739076941956816589)
XLA Ops:
  20.1 9.4 bitcast_dynamic-update-slice_fusion
  29.5 4.8 multiply_sine_fusion
  38.3 22.7 %qkv.5 = (bf16[4,1024,256]{2,1,0:T(8,128)(2,1)}, bf16[4,2,256,256]{3,2,1,0:T(8,128)(2,1)}) custom-call(bf16[256,4096]{1,0:T(8,128)(2,1)} %norm.4.refs_2_.refs_0_, bf16[256,4096]{1,0:T(8,128)(2,1)} %norm.5.refs_2_.refs_1_, bf16[256,4096]{1,0:T(8,128)(2,1)} %norm.6.refs_2_, bf16[256,4096]{1,0:T(8,128)(2,1)} %norm.7.refs_3_, ...), custom_call_target="tpu_custom_call" | custom-call | flops 12884901888 | bytes 20971520 | tf_op jit(solution)/shard_map/qkv/pallas_call | solution.py:120
  61.1 22.7 %qkv.6 = (bf16[4,1024,256]{2,1,0:T(8,128)(2,1)}, bf16[4,2,256,256]{3,2,1,0:T(8,128)(2,1)}) custom-call(bf16[256,4096]{1,0:T(8,128)(2,1)} %collective-permute-done.refs_0_, bf16[256,4096]{1,0:T(8,128)(2,1)} %collective-permute-done.1.refs_1_, bf16[256,4096]{1,0:T(8,128)(2,1)} %collective-permute-done.2.refs_2_, ...), custom_call_target="tpu_custom_call" | custom-call | flops 12884901888 | bytes 20971520 | tf_op jit(solution)/shard_map/qkv/pallas_call | solution.py:120
  88.3 14.4 %qkv.7 = (bf16[2,1024,256]{2,1,0:T(8,128)(2,1)}, bf16[2,2,256,256]{3,2,1,0:T(8,128)(2,1)}) custom-call(bf16[256,4096]{1,0:T(8,128)(2,1)} %collective-permute-done.4.refs_0_, bf16[256,4096]{1,0:T(8,128)(2,1)} %collective-permute-done.5.refs_1_, bf16[4096,1536]{1,0:T(8,128)(2,1)} %bitcast_dynamic-update-slice_fusion.1.refs_4_.refs_2_, ...), custom_call_target="tpu_custom_call" | custom-call | flops 6442450944 | bytes 16777216 | tf_op jit(solution)/shard_map/qkv/pallas_call | solution.py:120
  102.7 30.0 %collective-permute-done.6.refs_0_ = bf16[256,4096]{1,0:T(8,128)(2,1)} collective-permute-done((bf16[256,4096]{1,0:T(8,128)(2,1)}, bf16[256,4096]{1,0:T(8,128)(2,1)}, u32[]{:S(2)}, u32[]{:S(2)}) %collective-permute-start.6) | collective-permute-done | bytes 2097184 | tf_op jit(solution)/shard_map/ppermute | solution.py:624
  132.6 54.6 %flash_part.1.refs_7_.refs_14_ = f32[10,2,4,144,256]{4,3,2,1,0:T(8,128)} custom-call(s32[969]{0:T(1024)} %bitcast.28, bf16[4,1024,256]{2,1,0:T(8,128)(2,1)} %get-tuple-element.75.refs_1_, bf16[4,1024,256]{2,1,0:T(8,128)(2,1)} %get-tuple-element.77.refs_2_, bf16[2,1024,256]{2,1,0:T(8,128)(2,1)} %get-tuple-element.80.refs_3_, ...), custom_call_target="tpu_custom_call" | custom-call | flops 38654705664 | bytes 13107200 | tf_op jit(solution)/shard_map/flash_part/pallas_call | solution.py:336
  191.9 22.6 %qkv.8 = (bf16[4,1024,256]{2,1,0:T(8,128)(2,1)}, bf16[4,2,256,256]{3,2,1,0:T(8,128)(2,1)}) custom-call(bf16[256,4096]{1,0:T(8,128)(2,1)} %collective-permute-done.6.refs_0_, bf16[256,4096]{1,0:T(8,128)(2,1)} %collective-permute-done.7.refs_1_, bf16[256,4096]{1,0:T(8,128)(2,1)} %collective-permute-done.8.refs_2_, ...), custom_call_target="tpu_custom_call" | custom-call | flops 12884901888 | bytes 20971520 | tf_op jit(solution)/shard_map/qkv/pallas_call | solution.py:120
  214.5 21.1 %collective-permute-done.10.refs_0_ = bf16[256,4096]{1,0:T(8,128)(2,1)} collective-permute-done((bf16[256,4096]{1,0:T(8,128)(2,1)}, bf16[256,4096]{1,0:T(8,128)(2,1)}, u32[]{:S(2)}, u32[]{:S(2)}) %collective-permute-start.10) | collective-permute-done | bytes 2097184 | tf_op jit(solution)/shard_map/ppermute | solution.py:624
  244.3 14.1 %qkv.9 = (bf16[2,1024,256]{2,1,0:T(8,128)(2,1)}, bf16[2,2,256,256]{3,2,1,0:T(8,128)(2,1)}) custom-call(bf16[256,4096]{1,0:T(8,128)(2,1)} %collective-permute-done.10.refs_0_, bf16[256,4096]{1,0:T(8,128)(2,1)} %collective-permute-done.11.refs_1_, bf16[4096,1536]{1,0:T(8,128)(2,1)} %bitcast_dynamic-update-slice_fusion.1.refs_4_.refs_2_, ...), custom_call_target="tpu_custom_call" | custom-call | flops 6442450944 | bytes 16777216 | tf_op jit(solution)/shard_map/qkv/pallas_call | solution.py:120
  258.4 7.4 collective-permute-done.24.refs_10_
  267.4 21.7 %collective-permute-done.13.refs_10_ = bf16[4,2,256,256]{3,2,1,0:T(8,128)(2,1)} collective-permute-done((bf16[4,2,256,256]{3,2,1,0:T(8,128)(2,1)}, bf16[4,2,256,256]{3,2,1,0:T(8,128)(2,1)}, u32[]{:S(2)}, u32[]{:S(2)}) %collective-permute-start.13) | collective-permute-done | bytes 1048608 | tf_op jit(solution)/shard_map/ppermute | solution.py:624
  290.8 9.5 collective-permute-done.14.refs_11_
  302.0 20.7 %collective-permute-done.15.refs_12_ = bf16[4,2,256,256]{3,2,1,0:T(8,128)(2,1)} collective-permute-done((bf16[4,2,256,256]{3,2,1,0:T(8,128)(2,1)}, bf16[4,2,256,256]{3,2,1,0:T(8,128)(2,1)}, u32[]{:S(2)}, u32[]{:S(2)}) %collective-permute-start.15) | collective-permute-done | bytes 1048608 | tf_op jit(solution)/shard_map/ppermute | solution.py:624
  324.5 8.9 collective-permute-done.16.refs_13_
  333.4 30.2 %flash.4 = (bf16[256,1024]{1,0:T(8,128)(2,1)}, bf16[256,1024]{1,0:T(8,128)(2,1)}, bf16[256,1024]{1,0:T(8,128)(2,1)}, bf16[256,1024]{1,0:T(8,128)(2,1)}) custom-call(s32[969]{0:T(1024)} %bitcast.29, bf16[4,1024,256]{2,1,0:T(8,128)(2,1)} %get-tuple-element.75.refs_1_, bf16[4,1024,256]{2,1,0:T(8,128)(2,1)} %get-tuple-element.77.refs_2_, ...), custom_call_target="tpu_custom_call" | custom-call | flops 27917287424 | bytes 12582912 | tf_op jit(solution)/shard_map/flash/pallas_call | solution.py:336
  365.5 11.6 collective-permute-start.18
  377.1 44.3 %flash.5 = (bf16[256,1024]{1,0:T(8,128)(2,1)}, bf16[256,1024]{1,0:T(8,128)(2,1)}, bf16[256,1024]{1,0:T(8,128)(2,1)}, bf16[256,1024]{1,0:T(8,128)(2,1)}) custom-call(s32[969]{0:T(1024)} %bitcast.30, bf16[4,1024,256]{2,1,0:T(8,128)(2,1)} %get-tuple-element.75.refs_1_, bf16[4,1024,256]{2,1,0:T(8,128)(2,1)} %get-tuple-element.77.refs_2_, ...), custom_call_target="tpu_custom_call" | custom-call | flops 32212254720 | bytes 12582912 | tf_op jit(solution)/shard_map/flash/pallas_call | solution.py:336
  427.5 11.7 collective-permute-done.21.refs_6_
  439.1 8.8 collective-permute-done.29.refs_15_
  448.0 22.5 %collective-permute-done.30.refs_16_ = bf16[128,4096]{1,0:T(8,128)(2,1)} collective-permute-done((bf16[128,4096]{1,0:T(8,128)(2,1)}, bf16[128,4096]{1,0:T(8,128)(2,1)}, u32[]{:S(2)}, u32[]{:S(2)}) %collective-permute-start.30) | collective-permute-done | bytes 1048608 | tf_op jit(solution)/shard_map/ppermute | solution.py:624
  470.4 21.9 %collective-permute-done.31.refs_17_ = bf16[128,4096]{1,0:T(8,128)(2,1)} collective-permute-done((bf16[128,4096]{1,0:T(8,128)(2,1)}, bf16[128,4096]{1,0:T(8,128)(2,1)}, u32[]{:S(2)}, u32[]{:S(2)}) %collective-permute-start.31) | collective-permute-done | bytes 1048608 | tf_op jit(solution)/shard_map/ppermute | solution.py:624
  493.6 43.9 %flash.6 = (bf16[256,1024]{1,0:T(8,128)(2,1)}, bf16[256,1024]{1,0:T(8,128)(2,1)}, bf16[256,1024]{1,0:T(8,128)(2,1)}, bf16[256,1024]{1,0:T(8,128)(2,1)}) custom-call(s32[969]{0:T(1024)} %bitcast.31, bf16[4,1024,256]{2,1,0:T(8,128)(2,1)} %get-tuple-element.75.refs_1_, bf16[4,1024,256]{2,1,0:T(8,128)(2,1)} %get-tuple-element.77.refs_2_, ...), custom_call_target="tpu_custom_call" | custom-call | flops 32212254720 | bytes 12582912 | tf_op jit(solution)/shard_map/flash/pallas_call | solution.py:336
  546.0 31.5 %outp.2 = (bf16[256,4096]{1,0:T(8,128)(2,1)}, bf16[256,4096]{1,0:T(8,128)(2,1)}, bf16[256,4096]{1,0:T(8,128)(2,1)}, bf16[256,4096]{1,0:T(8,128)(2,1)}) custom-call(bf16[256,1024]{1,0:T(8,128)(2,1)} %get-tuple-element.87.refs_15_.refs_0_, bf16[256,1024]{1,0:T(8,128)(2,1)} %collective-permute-done.17.refs_1_, ...), custom_call_target="tpu_custom_call" | custom-call | flops 17179869184 | bytes 50331648 | tf_op jit(solution)/shard_map/outp/pallas_call | solution.py:430
  578.8 43.5 %flash.7 = (bf16[256,1024]{1,0:T(8,128)(2,1)}, bf16[256,1024]{1,0:T(8,128)(2,1)}, bf16[256,1024]{1,0:T(8,128)(2,1)}, bf16[256,1024]{1,0:T(8,128)(2,1)}) custom-call(s32[969]{0:T(1024)} %bitcast.32, bf16[4,1024,256]{2,1,0:T(8,128)(2,1)} %get-tuple-element.75.refs_1_, bf16[4,1024,256]{2,1,0:T(8,128)(2,1)} %get-tuple-element.77.refs_2_, ...), custom_call_target="tpu_custom_call" | custom-call | flops 32212254720 | bytes 12582912 | tf_op jit(solution)/shard_map/flash/pallas_call | solution.py:336
  630.4 90.0 %mlp.4 = (bf16[512,4096]{1,0:T(8,128)(2,1)}, bf16[512,4096]{1,0:T(8,128)(2,1)}) custom-call(bf16[256,4096]{1,0:T(8,128)(2,1)} %get-tuple-element.106.refs_0_, bf16[256,4096]{1,0:T(8,128)(2,1)} %collective-permute-done.40.refs_1_, bf16[256,4096]{1,0:T(8,128)(2,1)} %collective-permute-done.41.refs_2_, bf16[256,4096]{1,0:T(8,128)(2,1)} %collective-permute-done.42.refs_3_, ...), custom_call_target="tpu_custom_call" | custom-call | flops 77309411328 | bytes 92274688 | tf_op jit(solution)/shard_map/mlp/pallas_call | solution.py:487
  722.4 6.3 collective-permute-done.44.refs_1_
  728.8 7.2 collective-permute-done.45.refs_2_
  737.2 8.7 collective-permute-done.46.refs_3_
  747.1 11.4 collective-permute-done.48.refs_6_
  758.5 9.6 collective-permute-done.49.refs_7_
  768.1 31.6 %outp.3 = (bf16[256,4096]{1,0:T(8,128)(2,1)}, bf16[256,4096]{1,0:T(8,128)(2,1)}, bf16[256,4096]{1,0:T(8,128)(2,1)}, bf16[256,4096]{1,0:T(8,128)(2,1)}) custom-call(bf16[256,1024]{1,0:T(8,128)(2,1)} %get-tuple-element.103.refs_28_.refs_0_, bf16[256,1024]{1,0:T(8,128)(2,1)} %collective-permute-done.44.refs_1_, ...), custom_call_target="tpu_custom_call" | custom-call | flops 17179869184 | bytes 50331648 | tf_op jit(solution)/shard_map/outp/pallas_call | solution.py:430
  804.0 90.2 %mlp.5 = (bf16[512,4096]{1,0:T(8,128)(2,1)}, bf16[512,4096]{1,0:T(8,128)(2,1)}) custom-call(bf16[256,4096]{1,0:T(8,128)(2,1)} %get-tuple-element.122.refs_0_, bf16[256,4096]{1,0:T(8,128)(2,1)} %collective-permute-done.52.refs_1_, bf16[256,4096]{1,0:T(8,128)(2,1)} %collective-permute-done.53.refs_2_, bf16[256,4096]{1,0:T(8,128)(2,1)} %collective-permute-done.54.refs_3_, ...), custom_call_target="tpu_custom_call" | custom-call | flops 77309411328 | bytes 92274688 | tf_op jit(solution)/shard_map/mlp/pallas_call | solution.py:487
  896.0 46.7 %collective-permute-done.51.refs_1_ = bf16[256,4096]{1,0:T(8,128)(2,1)S(1)} collective-permute-done((bf16[256,4096]{1,0:T(8,128)(2,1)}, bf16[256,4096]{1,0:T(8,128)(2,1)S(1)}, u32[]{:S(2)}, u32[]{:S(2)}) %collective-permute-start.51) | collective-permute-done | bytes 2097184 | tf_op jit(solution)/shard_map/ppermute | solution.py:624
  942.7 5.3 add_convert_fusion.2.refs_7_
  949.3 90.1 %mlp.6 = (bf16[512,4096]{1,0:T(8,128)(2,1)}, bf16[512,4096]{1,0:T(8,128)(2,1)}) custom-call(bf16[256,4096]{1,0:T(8,128)(2,1)} %get-tuple-element.121.refs_0_, bf16[256,4096]{1,0:T(8,128)(2,1)} %copy-done.3, bf16[256,4096]{1,0:T(8,128)(2,1)} %copy-done.4, bf16[256,4096]{1,0:T(8,128)(2,1)} %collective-permute-done.56.refs_3_, bf16[4096,3072]{1,0:T(8,128)(2,1)} %refs_4_.7, ...), custom_call_target="tpu_custom_call" | custom-call | flops 77309411328 | bytes 92274688 | tf_op jit(solution)/shard_map/mlp/pallas_call | solution.py:487
  1041.8 46.8 %collective-permute-done.59.refs_1_ = bf16[256,4096]{1,0:T(8,128)(2,1)} collective-permute-done((bf16[256,4096]{1,0:T(8,128)(2,1)}, bf16[256,4096]{1,0:T(8,128)(2,1)}, u32[]{:S(2)}, u32[]{:S(2)}) %collective-permute-start.59) | collective-permute-done | bytes 2097184 | tf_op jit(solution)/shard_map/ppermute | solution.py:624
  1088.6 44.1 %collective-permute-done.50.refs_2_ = bf16[256,4096]{1,0:T(8,128)(2,1)} collective-permute-done((bf16[256,4096]{1,0:T(8,128)(2,1)}, bf16[256,4096]{1,0:T(8,128)(2,1)}, u32[]{:S(2)}, u32[]{:S(2)}) %collective-permute-start.50) | collective-permute-done | bytes 2097184 | tf_op jit(solution)/shard_map/ppermute | solution.py:624
  1132.7 5.6 zsum.4.refs_0_
  1138.2 4.3 add_convert_fusion.1.refs_7_
  1142.5 90.3 %mlp.7 = (bf16[512,4096]{1,0:T(8,128)(2,1)}, bf16[512,4096]{1,0:T(8,128)(2,1)}) custom-call(bf16[256,4096]{1,0:T(8,128)(2,1)} %get-tuple-element.129.refs_0_, bf16[256,4096]{1,0:T(8,128)(2,1)} %collective-permute-done.59.refs_1_, bf16[256,4096]{1,0:T(8,128)(2,1)} %collective-permute-done.60.refs_2_, bf16[256,4096]{1,0:T(8,128)(2,1)} %collective-permute-done.61.refs_3_, ...), custom_call_target="tpu_custom_call" | custom-call | flops 77309411328 | bytes 92274688 | tf_op jit(solution)/shard_map/mlp/pallas_call | solution.py:487
  1234.9 46.8 %collective-permute-done.58.refs_3_ = bf16[256,4096]{1,0:T(8,128)(2,1)} collective-permute-done((bf16[256,4096]{1,0:T(8,128)(2,1)}, bf16[256,4096]{1,0:T(8,128)(2,1)}, u32[]{:S(2)}, u32[]{:S(2)}) %collective-permute-start.58) | collective-permute-done | bytes 2097184 | tf_op jit(solution)/shard_map/ppermute | solution.py:624
  1281.7 5.6 zsum.5.refs_0_
  1287.3 4.4 add_convert_fusion.refs_5_
  1292.7 33.9 %collective-permute-done.63.refs_3_ = bf16[256,4096]{1,0:T(8,128)(2,1)} collective-permute-done((bf16[256,4096]{1,0:T(8,128)(2,1)}, bf16[256,4096]{1,0:T(8,128)(2,1)}, u32[]{:S(2)}, u32[]{:S(2)}) %collective-permute-start.63) | collective-permute-done | bytes 2097184 | tf_op jit(solution)/shard_map/ppermute | solution.py:624
  1326.7 5.6 zsum.6.refs_0_
  1332.3 38.9 %collective-permute-done.65.refs_3_ = bf16[256,4096]{1,0:T(8,128)(2,1)} collective-permute-done((bf16[256,4096]{1,0:T(8,128)(2,1)}, bf16[256,4096]{1,0:T(8,128)(2,1)}, u32[]{:S(2)}, u32[]{:S(2)}) %collective-permute-start.65) | collective-permute-done | bytes 2097184 | tf_op jit(solution)/shard_map/ppermute | solution.py:624
  1371.1 5.6 zsum.7
  (133 shorter events, 93.3 us)
Async XLA Ops:
  4.7 79.0 %collective-permute-start.4 = (bf16[256,4096]{1,0:T(8,128)(2,1)}, bf16[256,4096]{1,0:T(8,128)(2,1)}, u32[]{:S(2)}, u32[]{:S(2)}) collective-permute-start(bf16[256,4096]{1,0:T(8,128)(2,1)} %norm.4.refs_2_.refs_0_), channel_id=1, source_target_pairs={{0,2},{1,3},{2,0},{3,1},{4,6},{5,7},{6,4},{7,5}} | collective-permute-start | bytes 6291464 | tf_op jit(solution)/shard_map/ppermute | solution.py:624
  8.0 53.1 %collective-permute-start = (bf16[256,4096]{1,0:T(8,128)(2,1)}, bf16[256,4096]{1,0:T(8,128)(2,1)}, u32[]{:S(2)}, u32[]{:S(2)}) collective-permute-start(bf16[256,4096]{1,0:T(8,128)(2,1)} %norm.4.refs_2_.refs_0_), channel_id=1, source_target_pairs={{0,1},{1,0},{2,3},{3,2},{4,5},{5,4},{6,7},{7,6}} | collective-permute-start | bytes 6291464 | tf_op jit(solution)/shard_map/ppermute | solution.py:624
  11.4 49.6 %collective-permute-start.1 = (bf16[256,4096]{1,0:T(8,128)(2,1)}, bf16[256,4096]{1,0:T(8,128)(2,1)}, u32[]{:S(2)}, u32[]{:S(2)}) collective-permute-start(bf16[256,4096]{1,0:T(8,128)(2,1)} %norm.5.refs_2_.refs_1_), channel_id=1, source_target_pairs={{0,1},{1,0},{2,3},{3,2},{4,5},{5,4},{6,7},{7,6}} | collective-permute-start | bytes 6291464 | tf_op jit(solution)/shard_map/ppermute | solution.py:624
  15.3 45.7 %collective-permute-start.2 = (bf16[256,4096]{1,0:T(8,128)(2,1)}, bf16[256,4096]{1,0:T(8,128)(2,1)}, u32[]{:S(2)}, u32[]{:S(2)}) collective-permute-start(bf16[256,4096]{1,0:T(8,128)(2,1)} %norm.6.refs_2_), channel_id=1, source_target_pairs={{0,1},{1,0},{2,3},{3,2},{4,5},{5,4},{6,7},{7,6}} | collective-permute-start | bytes 6291464 | tf_op jit(solution)/shard_map/ppermute | solution.py:624
  18.8 42.2 %collective-permute-start.3 = (bf16[256,4096]{1,0:T(8,128)(2,1)}, bf16[256,4096]{1,0:T(8,128)(2,1)}, u32[]{:S(2)}, u32[]{:S(2)}) collective-permute-start(bf16[256,4096]{1,0:T(8,128)(2,1)} %norm.7.refs_3_), channel_id=1, source_target_pairs={{0,1},{1,0},{2,3},{3,2},{4,5},{5,4},{6,7},{7,6}} | collective-permute-start | bytes 6291464 | tf_op jit(solution)/shard_map/ppermute | solution.py:624
  83.8 48.8 %collective-permute-start.6 = (bf16[256,4096]{1,0:T(8,128)(2,1)}, bf16[256,4096]{1,0:T(8,128)(2,1)}, u32[]{:S(2)}, u32[]{:S(2)}) collective-permute-start(bf16[256,4096]{1,0:T(8,128)(2,1)} %norm.5.refs_2_.refs_1_), channel_id=1, source_target_pairs={{0,2},{1,3},{2,0},{3,1},{4,6},{5,7},{6,4},{7,5}} | collective-permute-start | bytes 6291464 | tf_op jit(solution)/shard_map/ppermute | solution.py:624
  83.8 103.4 %collective-permute-start.8 = (bf16[256,4096]{1,0:T(8,128)(2,1)}, bf16[256,4096]{1,0:T(8,128)(2,1)}, u32[]{:S(2)}, u32[]{:S(2)}) collective-permute-start(bf16[256,4096]{1,0:T(8,128)(2,1)} %norm.6.refs_2_), channel_id=1, source_target_pairs={{0,2},{1,3},{2,0},{3,1},{4,6},{5,7},{6,4},{7,5}} | collective-permute-start | bytes 6291464 | tf_op jit(solution)/shard_map/ppermute | solution.py:624
  132.6 55.1 %collective-permute-start.7 = (bf16[256,4096]{1,0:T(8,128)(2,1)}, bf16[256,4096]{1,0:T(8,128)(2,1)}, u32[]{:S(2)}, u32[]{:S(2)}) collective-permute-start(bf16[256,4096]{1,0:T(8,128)(2,1)} %collective-permute-done.6.refs_0_), channel_id=1, source_target_pairs={{0,1},{1,0},{2,3},{3,2},{4,5},{5,4},{6,7},{7,6}} | collective-permute-start | bytes 6291464 | tf_op jit(solution)/shard_map/ppermute | solution.py:624
  187.8 47.9 %collective-permute-start.10 = (bf16[256,4096]{1,0:T(8,128)(2,1)}, bf16[256,4096]{1,0:T(8,128)(2,1)}, u32[]{:S(2)}, u32[]{:S(2)}) collective-permute-start(bf16[256,4096]{1,0:T(8,128)(2,1)} %norm.7.refs_3_), channel_id=1, source_target_pairs={{0,2},{1,3},{2,0},{3,1},{4,6},{5,7},{6,4},{7,5}} | collective-permute-start | bytes 6291464 | tf_op jit(solution)/shard_map/ppermute | solution.py:624
  240.2 27.1 %collective-permute-start.12 = (bf16[4,2,256,256]{3,2,1,0:T(8,128)(2,1)}, bf16[4,2,256,256]{3,2,1,0:T(8,128)(2,1)}, u32[]{:S(2)}, u32[]{:S(2)}) collective-permute-start(bf16[4,2,256,256]{3,2,1,0:T(8,128)(2,1)} %get-tuple-element.76.refs_7_.refs_4_), channel_id=1, source_target_pairs={{0,4},{4,0},{1,5},{5,1},{2,6},{6,2},{3,7},{7,3}} | collective-permute-start | bytes 3145736 | tf_op jit(solution)/shard_map/ppermute | solution.py:624
  242.1 47.0 %collective-permute-start.13 = (bf16[4,2,256,256]{3,2,1,0:T(8,128)(2,1)}, bf16[4,2,256,256]{3,2,1,0:T(8,128)(2,1)}, u32[]{:S(2)}, u32[]{:S(2)}) collective-permute-start(bf16[4,2,256,256]{3,2,1,0:T(8,128)(2,1)} %get-tuple-element.78.refs_5_), channel_id=1, source_target_pairs={{0,4},{4,0},{1,5},{5,1},{2,6},{6,2},{3,7},{7,3}} | collective-permute-start | bytes 3145736 | tf_op jit(solution)/shard_map/ppermute | solution.py:624
  242.3 58.0 %collective-permute-start.14 = (bf16[2,2,256,256]{3,2,1,0:T(8,128)(2,1)}, bf16[2,2,256,256]{3,2,1,0:T(8,128)(2,1)}, u32[]{:S(2)}, u32[]{:S(2)}) collective-permute-start(bf16[2,2,256,256]{3,2,1,0:T(8,128)(2,1)} %get-tuple-element.81.refs_6_), channel_id=1, source_target_pairs={{0,4},{4,0},{1,5},{5,1},{2,6},{6,2},{3,7},{7,3}} | collective-permute-start | bytes 1572872 | tf_op jit(solution)/shard_map/ppermute | solution.py:624
  244.1 78.6 %collective-permute-start.15 = (bf16[4,2,256,256]{3,2,1,0:T(8,128)(2,1)}, bf16[4,2,256,256]{3,2,1,0:T(8,128)(2,1)}, u32[]{:S(2)}, u32[]{:S(2)}) collective-permute-start(bf16[4,2,256,256]{3,2,1,0:T(8,128)(2,1)} %get-tuple-element.84.refs_5_.refs_7_), channel_id=1, source_target_pairs={{0,4},{4,0},{1,5},{5,1},{2,6},{6,2},{3,7},{7,3}} | collective-permute-start | bytes 3145736 | tf_op jit(solution)/shard_map/ppermute | solution.py:624
  265.8 67.5 %collective-permute-start.16 = (bf16[2,2,256,256]{3,2,1,0:T(8,128)(2,1)}, bf16[2,2,256,256]{3,2,1,0:T(8,128)(2,1)}, u32[]{:S(2)}, u32[]{:S(2)}) collective-permute-start(bf16[2,2,256,256]{3,2,1,0:T(8,128)(2,1)} %get-tuple-element.86.refs_8_.refs_15_), channel_id=1, source_target_pairs={{0,4},{4,0},{1,5},{5,1},{2,6},{6,2},{3,7},{7,3}} | collective-permute-start | bytes 1572872 | tf_op jit(solution)/shard_map/ppermute | solution.py:624
  267.3 278.7 %collective-permute-start.23 = (bf16[1024,4096]{1,0:T(8,128)(2,1)}, bf16[1024,4096]{1,0:T(8,128)(2,1)}, u32[]{:S(2)}, u32[]{:S(2)}) collective-permute-start(bf16[1024,4096]{1,0:T(8,128)(2,1)} %bitcast.23), channel_id=1, source_target_pairs={{0,1},{1,0},{2,3},{3,2},{4,5},{5,4},{6,7},{7,6}} | collective-permute-start | bytes 25165832 | tf_op jit(solution)/shard_map/ppermute | solution.py:624
  289.0 74.6 %collective-permute-start.27 = (bf16[128,4096]{1,0:T(8,128)(2,1)}, bf16[128,4096]{1,0:T(8,128)(2,1)}, u32[]{:S(2)}, u32[]{:S(2)}) collective-permute-start(bf16[128,4096]{1,0:T(8,128)(2,1)} %get-tuple-element.137), channel_id=1, source_target_pairs={{0,2},{1,3},{2,0},{3,1},{4,6},{5,7},{6,4},{7,5}} | collective-permute-start | bytes 3145736 | tf_op jit(solution)/shard_map/ppermute | solution.py:624
  300.3 65.0 %collective-permute-start.26 = (bf16[128,4096]{1,0:T(8,128)(2,1)}, bf16[128,4096]{1,0:T(8,128)(2,1)}, u32[]{:S(2)}, u32[]{:S(2)}) collective-permute-start(bf16[128,4096]{1,0:T(8,128)(2,1)} %get-tuple-element.138), channel_id=1, source_target_pairs={{0,2},{1,3},{2,0},{3,1},{4,6},{5,7},{6,4},{7,5}} | collective-permute-start | bytes 3145736 | tf_op jit(solution)/shard_map/ppermute | solution.py:624
  322.8 42.8 %collective-permute-start.25 = (bf16[128,4096]{1,0:T(8,128)(2,1)}, bf16[128,4096]{1,0:T(8,128)(2,1)}, u32[]{:S(2)}, u32[]{:S(2)}) collective-permute-start(bf16[128,4096]{1,0:T(8,128)(2,1)} %get-tuple-element.139), channel_id=1, source_target_pairs={{0,2},{1,3},{2,0},{3,1},{4,6},{5,7},{6,4},{7,5}} | collective-permute-start | bytes 3145736 | tf_op jit(solution)/shard_map/ppermute | solution.py:624
  333.4 43.7 %collective-permute-start.32 = (bf16[128,4096]{1,0:T(8,128)(2,1)}, bf16[128,4096]{1,0:T(8,128)(2,1)}, u32[]{:S(2)}, u32[]{:S(2)}) collective-permute-start(bf16[128,4096]{1,0:T(8,128)(2,1)} %collective-permute-done.24.refs_10_), channel_id=1, source_target_pairs={{0,1},{1,0},{2,3},{3,2},{4,5},{5,4},{6,7},{7,6}} | collective-permute-start | bytes 3145736 | tf_op jit(solution)/shard_map/ppermute | solution.py:624
  363.6 57.8 %collective-permute-start.28 = (bf16[128,4096]{1,0:T(8,128)(2,1)}, bf16[128,4096]{1,0:T(8,128)(2,1)}, u32[]{:S(2)}, u32[]{:S(2)}) collective-permute-start(bf16[128,4096]{1,0:T(8,128)(2,1)} %collective-permute-done.24.refs_10_), channel_id=1, source_target_pairs={{0,4},{4,0},{1,5},{5,1},{2,6},{6,2},{3,7},{7,3}} | collective-permute-start | bytes 3145736 | tf_op jit(solution)/shard_map/ppermute | solution.py:624
  365.3 56.3 %collective-permute-start.17 = (bf16[256,1024]{1,0:T(8,128)(2,1)}, bf16[256,1024]{1,0:T(8,128)(2,1)}, u32[]{:S(2)}, u32[]{:S(2)}) collective-permute-start(bf16[256,1024]{1,0:T(8,128)(2,1)} %get-tuple-element.88), channel_id=1, source_target_pairs={{0,1},{1,0},{2,3},{3,2},{4,5},{5,4},{6,7},{7,6}} | collective-permute-start | bytes 1572872 | tf_op jit(solution)/shard_map/ppermute | solution.py:624
  365.5 56.8 %collective-permute-start.18 = (bf16[256,1024]{1,0:T(8,128)(2,1)}, bf16[256,1024]{1,0:T(8,128)(2,1)}, u32[]{:S(2)}, u32[]{:S(2)}) collective-permute-start(bf16[256,1024]{1,0:T(8,128)(2,1)} %get-tuple-element.89), channel_id=1, source_target_pairs={{0,2},{1,3},{2,0},{3,1},{4,6},{5,7},{6,4},{7,5}} | collective-permute-start | bytes 1572872 | tf_op jit(solution)/shard_map/ppermute | solution.py:624
  377.1 46.5 %collective-permute-start.19 = (bf16[256,1024]{1,0:T(8,128)(2,1)}, bf16[256,1024]{1,0:T(8,128)(2,1)}, u32[]{:S(2)}, u32[]{:S(2)}) collective-permute-start(bf16[256,1024]{1,0:T(8,128)(2,1)} %get-tuple-element.90), channel_id=1, source_target_pairs={{0,3},{1,2},{2,1},{3,0},{4,7},{5,6},{6,5},{7,4}} | collective-permute-start | bytes 1572872 | tf_op jit(solution)/shard_map/ppermute | solution.py:624
  422.4 48.0 %collective-permute-start.30 = (bf16[128,4096]{1,0:T(8,128)(2,1)}, bf16[128,4096]{1,0:T(8,128)(2,1)}, u32[]{:S(2)}, u32[]{:S(2)}) collective-permute-start(bf16[128,4096]{1,0:T(8,128)(2,1)} %collective-permute-done.26.refs_12_), channel_id=1, source_target_pairs={{0,4},{4,0},{1,5},{5,1},{2,6},{6,2},{3,7},{7,3}} | collective-permute-start | bytes 3145736 | tf_op jit(solution)/shard_map/ppermute | solution.py:624
  423.6 68.7 %collective-permute-start.31 = (bf16[128,4096]{1,0:T(8,128)(2,1)}, bf16[128,4096]{1,0:T(8,128)(2,1)}, u32[]{:S(2)}, u32[]{:S(2)}) collective-permute-start(bf16[128,4096]{1,0:T(8,128)(2,1)} %collective-permute-done.27.refs_13_), channel_id=1, source_target_pairs={{0,4},{4,0},{1,5},{5,1},{2,6},{6,2},{3,7},{7,3}} | collective-permute-start | bytes 3145736 | tf_op jit(solution)/shard_map/ppermute | solution.py:624
  439.1 99.8 %collective-permute-start.33 = (bf16[128,4096]{1,0:T(8,128)(2,1)}, bf16[128,4096]{1,0:T(8,128)(2,1)}, u32[]{:S(2)}, u32[]{:S(2)}) collective-permute-start(bf16[128,4096]{1,0:T(8,128)(2,1)} %collective-permute-done.25.refs_11_), channel_id=1, source_target_pairs={{0,1},{1,0},{2,3},{3,2},{4,5},{5,4},{6,7},{7,6}} | collective-permute-start | bytes 3145736 | tf_op jit(solution)/shard_map/ppermute | solution.py:624
  447.9 91.0 %collective-permute-start.34 = (bf16[128,4096]{1,0:T(8,128)(2,1)}, bf16[128,4096]{1,0:T(8,128)(2,1)}, u32[]{:S(2)}, u32[]{:S(2)}) collective-permute-start(bf16[128,4096]{1,0:T(8,128)(2,1)} %collective-permute-done.26.refs_12_), channel_id=1, source_target_pairs={{0,1},{1,0},{2,3},{3,2},{4,5},{5,4},{6,7},{7,6}} | collective-permute-start | bytes 3145736 | tf_op jit(solution)/shard_map/ppermute | solution.py:624
  470.4 69.0 %collective-permute-start.35 = (bf16[128,4096]{1,0:T(8,128)(2,1)}, bf16[128,4096]{1,0:T(8,128)(2,1)}, u32[]{:S(2)}, u32[]{:S(2)}) collective-permute-start(bf16[128,4096]{1,0:T(8,128)(2,1)} %collective-permute-done.27.refs_13_), channel_id=1, source_target_pairs={{0,1},{1,0},{2,3},{3,2},{4,5},{5,4},{6,7},{7,6}} | collective-permute-start | bytes 3145736 | tf_op jit(solution)/shard_map/ppermute | solution.py:624
  492.3 45.2 %collective-permute-start.22 = (bf16[256,1024]{1,0:T(8,128)(2,1)}, bf16[256,1024]{1,0:T(8,128)(2,1)}, u32[]{:S(2)}, u32[]{:S(2)}) collective-permute-start(bf16[256,1024]{1,0:T(8,128)(2,1)} %get-tuple-element.95), channel_id=1, source_target_pairs={{0,3},{1,2},{2,1},{3,0},{4,7},{5,6},{6,5},{7,4}} | collective-permute-start | bytes 1572872 | tf_op jit(solution)/shard_map/ppermute | solution.py:624
  577.6 49.5 %collective-permute-start.41 = (bf16[256,4096]{1,0:T(8,128)(2,1)}, bf16[256,4096]{1,0:T(8,128)(2,1)}, u32[]{:S(2)}, u32[]{:S(2)}) collective-permute-start(bf16[256,4096]{1,0:T(8,128)(2,1)} %get-tuple-element.106.refs_0_), channel_id=1, source_target_pairs={{0,1},{1,0},{2,3},{3,2},{4,5},{5,4},{6,7},{7,6}} | collective-permute-start | bytes 6291464 | tf_op jit(solution)/shard_map/ppermute | solution.py:624
  577.9 48.0 %collective-permute-start.40 = (bf16[256,4096]{1,0:T(8,128)(2,1)}, bf16[256,4096]{1,0:T(8,128)(2,1)}, u32[]{:S(2)}, u32[]{:S(2)}) collective-permute-start(bf16[256,4096]{1,0:T(8,128)(2,1)} %get-tuple-element.106.refs_0_), channel_id=1, source_target_pairs={{0,2},{1,3},{2,0},{3,1},{4,6},{5,7},{6,4},{7,5}} | collective-permute-start | bytes 6291464 | tf_op jit(solution)/shard_map/ppermute | solution.py:624
  625.9 111.2 %collective-permute-start.52 = (bf16[256,4096]{1,0:T(8,128)(2,1)}, bf16[256,4096]{1,0:T(8,128)(2,1)}, u32[]{:S(2)}, u32[]{:S(2)}) collective-permute-start(bf16[256,4096]{1,0:T(8,128)(2,1)} %get-tuple-element.122.refs_0_), channel_id=1, source_target_pairs={{0,2},{1,3},{2,0},{3,1},{4,6},{5,7},{6,4},{7,5}} | collective-permute-start | bytes 6291464 | tf_op jit(solution)/shard_map/ppermute | solution.py:624
  720.4 79.2 %collective-permute-start.43 = (bf16[512,4096]{1,0:T(8,128)(2,1)}, bf16[512,4096]{1,0:T(8,128)(2,1)}, u32[]{:S(2)}, u32[]{:S(2)}) collective-permute-start(bf16[512,4096]{1,0:T(8,128)(2,1)} %get-tuple-element.112), channel_id=1, source_target_pairs={{0,1},{1,0},{2,3},{3,2},{4,5},{5,4},{6,7},{7,6}} | collective-permute-start | bytes 12582920 | tf_op jit(solution)/shard_map/ppermute | solution.py:624
  737.1 30.9 %collective-permute-start.49 = (bf16[256,1024]{1,0:T(8,128)(2,1)}, bf16[256,1024]{1,0:T(8,128)(2,1)}, u32[]{:S(2)}, u32[]{:S(2)}) collective-permute-start(bf16[256,1024]{1,0:T(8,128)(2,1)} %get-tuple-element.118), channel_id=1, source_target_pairs={{0,3},{1,2},{2,1},{3,0},{4,7},{5,6},{6,5},{7,4}} | collective-permute-start | bytes 1572872 | tf_op jit(solution)/shard_map/ppermute | solution.py:624
  745.9 58.1 %collective-permute-start.53 = (bf16[256,4096]{1,0:T(8,128)(2,1)}, bf16[256,4096]{1,0:T(8,128)(2,1)}, u32[]{:S(2)}, u32[]{:S(2)}) collective-permute-start(bf16[256,4096]{1,0:T(8,128)(2,1)} %get-tuple-element.122.refs_0_), channel_id=1, source_target_pairs={{0,1},{1,0},{2,3},{3,2},{4,5},{5,4},{6,7},{7,6}} | collective-permute-start | bytes 6291464 | tf_op jit(solution)/shard_map/ppermute | solution.py:624
  747.1 56.9 %collective-permute-start.54 = (bf16[256,4096]{1,0:T(8,128)(2,1)}, bf16[256,4096]{1,0:T(8,128)(2,1)}, u32[]{:S(2)}, u32[]{:S(2)}) collective-permute-start(bf16[256,4096]{1,0:T(8,128)(2,1)} %collective-permute-done.52.refs_1_), channel_id=1, source_target_pairs={{0,1},{1,0},{2,3},{3,2},{4,5},{5,4},{6,7},{7,6}} | collective-permute-start | bytes 6291464 | tf_op jit(solution)/shard_map/ppermute | solution.py:624
  894.2 48.5 %collective-permute-start.57 = (bf16[512,4096]{1,0:T(8,128)(2,1)}, bf16[512,4096]{1,0:T(8,128)(2,1)S(1)}, u32[]{:S(2)}, u32[]{:S(2)}) collective-permute-start(bf16[512,4096]{1,0:T(8,128)(2,1)} %get-tuple-element.126), channel_id=1, source_target_pairs={{0,1},{1,0},{2,3},{3,2},{4,5},{5,4},{6,7},{7,6}} | collective-permute-start | bytes 12582920 | tf_op jit(solution)/shard_map/ppermute | solution.py:624
  894.9 47.8 %collective-permute-start.51 = (bf16[256,4096]{1,0:T(8,128)(2,1)}, bf16[256,4096]{1,0:T(8,128)(2,1)S(1)}, u32[]{:S(2)}, u32[]{:S(2)}) collective-permute-start(bf16[256,4096]{1,0:T(8,128)(2,1)} %get-tuple-element.121.refs_0_), channel_id=1, source_target_pairs={{0,2},{1,3},{2,0},{3,1},{4,6},{5,7},{6,4},{7,5}} | collective-permute-start | bytes 6291464 | tf_op jit(solution)/shard_map/ppermute | solution.py:624
  896.0 52.0 %collective-permute-start.55 = (bf16[256,4096]{1,0:T(8,128)(2,1)}, bf16[256,4096]{1,0:T(8,128)(2,1)S(1)}, u32[]{:S(2)}, u32[]{:S(2)}) collective-permute-start(bf16[256,4096]{1,0:T(8,128)(2,1)} %get-tuple-element.121.refs_0_), channel_id=1, source_target_pairs={{0,1},{1,0},{2,3},{3,2},{4,5},{5,4},{6,7},{7,6}} | collective-permute-start | bytes 6291464 | tf_op jit(solution)/shard_map/ppermute | solution.py:624
  1039.3 98.9 %collective-permute-start.62 = (bf16[512,4096]{1,0:T(8,128)(2,1)}, bf16[512,4096]{1,0:T(8,128)(2,1)}, u32[]{:S(2)}, u32[]{:S(2)}) collective-permute-start(bf16[512,4096]{1,0:T(8,128)(2,1)} %get-tuple-element.132), channel_id=1, source_target_pairs={{0,1},{1,0},{2,3},{3,2},{4,5},{5,4},{6,7},{7,6}} | collective-permute-start | bytes 12582920 | tf_op jit(solution)/shard_map/ppermute | solution.py:624
  1039.8 48.8 %collective-permute-start.59 = (bf16[256,4096]{1,0:T(8,128)(2,1)}, bf16[256,4096]{1,0:T(8,128)(2,1)}, u32[]{:S(2)}, u32[]{:S(2)}) collective-permute-start(bf16[256,4096]{1,0:T(8,128)(2,1)} %get-tuple-element.129.refs_0_), channel_id=1, source_target_pairs={{0,2},{1,3},{2,0},{3,1},{4,6},{5,7},{6,4},{7,5}} | collective-permute-start | bytes 6291464 | tf_op jit(solution)/shard_map/ppermute | solution.py:624
  1040.9 91.8 %collective-permute-start.50 = (bf16[256,4096]{1,0:T(8,128)(2,1)}, bf16[256,4096]{1,0:T(8,128)(2,1)}, u32[]{:S(2)}, u32[]{:S(2)}) collective-permute-start(bf16[256,4096]{1,0:T(8,128)(2,1)} %add_convert_fusion.3.refs_7_), channel_id=1, source_target_pairs={{0,2},{1,3},{2,0},{3,1},{4,6},{5,7},{6,4},{7,5}} | collective-permute-start | bytes 6291464 | tf_op jit(solution)/shard_map/ppermute | solution.py:624
  1041.8 100.7 %collective-permute-start.60 = (bf16[256,4096]{1,0:T(8,128)(2,1)}, bf16[256,4096]{1,0:T(8,128)(2,1)}, u32[]{:S(2)}, u32[]{:S(2)}) collective-permute-start(bf16[256,4096]{1,0:T(8,128)(2,1)} %get-tuple-element.129.refs_0_), channel_id=1, source_target_pairs={{0,1},{1,0},{2,3},{3,2},{4,5},{5,4},{6,7},{7,6}} | collective-permute-start | bytes 6291464 | tf_op jit(solution)/shard_map/ppermute | solution.py:624
  1088.6 53.9 %collective-permute-start.61 = (bf16[256,4096]{1,0:T(8,128)(2,1)}, bf16[256,4096]{1,0:T(8,128)(2,1)}, u32[]{:S(2)}, u32[]{:S(2)}) collective-permute-start(bf16[256,4096]{1,0:T(8,128)(2,1)} %collective-permute-done.59.refs_1_), channel_id=1, source_target_pairs={{0,1},{1,0},{2,3},{3,2},{4,5},{5,4},{6,7},{7,6}} | collective-permute-start | bytes 6291464 | tf_op jit(solution)/shard_map/ppermute | solution.py:624
  1232.9 54.4 %collective-permute-start.64 = (bf16[512,4096]{1,0:T(8,128)(2,1)}, bf16[512,4096]{1,0:T(8,128)(2,1)}, u32[]{:S(2)}, u32[]{:S(2)}) collective-permute-start(bf16[512,4096]{1,0:T(8,128)(2,1)} %get-tuple-element.135), channel_id=1, source_target_pairs={{0,1},{1,0},{2,3},{3,2},{4,5},{5,4},{6,7},{7,6}} | collective-permute-start | bytes 12582920 | tf_op jit(solution)/shard_map/ppermute | solution.py:624
  1232.9 48.8 %collective-permute-start.58 = (bf16[256,4096]{1,0:T(8,128)(2,1)}, bf16[256,4096]{1,0:T(8,128)(2,1)}, u32[]{:S(2)}, u32[]{:S(2)}) collective-permute-start(bf16[256,4096]{1,0:T(8,128)(2,1)} %add_convert_fusion.2.refs_7_), channel_id=1, source_target_pairs={{0,2},{1,3},{2,0},{3,1},{4,6},{5,7},{6,4},{7,5}} | collective-permute-start | bytes 6291464 | tf_op jit(solution)/shard_map/ppermute | solution.py:624
  1234.0 92.7 %collective-permute-start.63 = (bf16[256,4096]{1,0:T(8,128)(2,1)}, bf16[256,4096]{1,0:T(8,128)(2,1)}, u32[]{:S(2)}, u32[]{:S(2)}) collective-permute-start(bf16[256,4096]{1,0:T(8,128)(2,1)} %add_convert_fusion.1.refs_7_), channel_id=1, source_target_pairs={{0,2},{1,3},{2,0},{3,1},{4,6},{5,7},{6,4},{7,5}} | collective-permute-start | bytes 6291464 | tf_op jit(solution)/shard_map/ppermute | solution.py:624
  1291.7 79.5 %collective-permute-start.65 = (bf16[256,4096]{1,0:T(8,128)(2,1)}, bf16[256,4096]{1,0:T(8,128)(2,1)}, u32[]{:S(2)}, u32[]{:S(2)}) collective-permute-start(bf16[256,4096]{1,0:T(8,128)(2,1)} %add_convert_fusion.refs_5_), channel_id=1, source_target_pairs={{0,2},{1,3},{2,0},{3,1},{4,6},{5,7},{6,4},{7,5}} | collective-permute-start | bytes 6291464 | tf_op jit(solution)/shard_map/ppermute | solution.py:624
  (23 other events, 225.6 us)

commit v6 on v5

--- a/solution.py
+++ b/solution.py
@@ -39,6 +39,10 @@
     return (f * lax.rsqrt(mean_sq + NORM_EPS) * gain.astype(F32)).astype(BF)
 
 
+def cost(flops, moved):
+    return pl.CostEstimate(flops=flops, transcendentals=0, bytes_accessed=moved)
+
+
 def ordered(kernel, n_in, after):
     n = len(after)
     return lambda *refs: kernel(*refs[:n_in], *refs[n_in + n:])
@@ -58,7 +62,7 @@
         out_specs=pl.BlockSpec((tile, dim), lambda i: (i, 0)),
         out_shape=jax.ShapeDtypeStruct((RUN, dim), BF),
         name="norm", compiler_params=params(1),
-        cost_estimate=pl.CostEstimate(flops=8 * RUN * dim, transcendentals=0, bytes_accessed=4 * RUN * dim),
+        cost_estimate=cost(RUN * dim, RUN * dim),
     )(x_rows, gain, *after)
 
 
@@ -126,8 +130,7 @@
         out_shape=[jax.ShapeDtypeStruct((n_in, n_q * tn, RUN), BF), jax.ShapeDtypeStruct((n_in, 2, 256, 256), BF)],
         scratch_shapes=[pltpu.VMEM((n_in * RUN, dim), BF), pltpu.SemaphoreType.DMA((n_in,))],
         name="qkv", compiler_params=params(1),
-        cost_estimate=pl.CostEstimate(flops=2 * n_in * RUN * w_all.size, transcendentals=0,
-                                      bytes_accessed=2 * (n_in * RUN * dim + w_all.size)),
+        cost_estimate=cost(2 * n_in * RUN * w_all.size, 2 * w_all.size),
     )(*rows, w_all, cos, sin, *after)
 
 
@@ -150,17 +153,19 @@
 
     q_copies = [pltpu.make_async_copy(qs[a].at[i], q_scr.at[t], q_sem.at[t]) for t, (a, i) in enumerate(q_src)]
     kv_copies = [pltpu.make_async_copy(kvs[a].at[i], kv_scr.at[r], kv_sem.at[r]) for r, (a, i) in enumerate(kv_src)]
-    for cp in q_copies:
+    first = 4
+    q_copies[0].start()
+    for cp in kv_copies[:first]:
+        cp.start()
+    for cp in q_copies[1:]:
         cp.start()
     for t, i in enumerate(st_src):
         if i is not None:
             @pl.when(tab_ref[carried + t] != 0)
             def _():
                 pltpu.make_async_copy(sts[0].at[i], st_scr.at[t], st_sem.at[t]).start()
-    for cp in kv_copies:
+    for cp in kv_copies[first:]:
         cp.start()
-    for cp in q_copies:
-        cp.wait()
 
     def block(i):
         g = lax.div(i, n_blocks)
@@ -240,6 +245,7 @@
             def _():
                 @pl.when(g == 0)
                 def _():
+                    pltpu.make_async_copy(q_scr.at[tile], q_scr.at[tile], q_sem.at[tile]).wait()
                     pltpu.make_async_copy(st_scr.at[tile], st_scr.at[tile], st_sem.at[tile]).wait()
 
                 finish(tile, g, lambda h: (st_scr[tile, g, h, :HD, :], st_scr[tile, g, h, HD + 8:, :]))
@@ -248,7 +254,12 @@
 
         lax.fori_loop(0, n_tiles * n_heads, idle, 0)
 
+    def query(row):
+        t = tab_ref[row]
+        pltpu.make_async_copy(q_scr.at[t], q_scr.at[t], q_sem.at[t]).wait()
+
     row, g = block(0)
+    query(row)
     have = arrived(0, tab_ref[row + 2])
     for h in range(G):
         stage_a(row, g, h)
@@ -259,6 +270,10 @@
         have = arrived(have, tab_ref[nrow + 2])
         flags = tab_ref[row + 1]
         tile = tab_ref[row]
+
+        @pl.when((i + 1 < n_blocks) & ((tab_ref[nrow + 1] & FIRST) != 0))
+        def _():
+            query(nrow)
 
         @pl.when((flags & (FIRST | CARRY)) == FIRST)
         def _():
@@ -358,143 +373,188 @@
         else [jax.ShapeDtypeStruct((st_tiles, *state), F32)],
         input_output_aliases={n_in - 1: 0} if sts and not final else {},
         name="flash" if final else "flash_part", compiler_params=pltpu.CompilerParams(vmem_limit_bytes=VMEM),
-        cost_estimate=pl.CostEstimate(flops=8 * work * RUN * RUN * nq, transcendentals=work * RUN * RUN * nq // HD,
-                                      bytes_accessed=n_runs * 2 * 256 * 256 * 2 + 4 * n_tiles * RUN * nq),
+        cost_estimate=cost(8 * work * RUN * RUN * nq, n_runs * RUN * nq),
     )(tab, *qs, *kvs, *sts, *after)
 
 
-def out_kernel(*refs, blocks, n_w, n_run):
-    n_o = 4 * n_run
+def out_kernel(*refs, blocks, n_w, n_run, at, parts):
+    n_o, n_out = 4 * n_run, 2 * len(parts)
     o_refs, w_refs, x_ref, g_ref = refs[:n_o], refs[n_o:n_o + n_w], refs[n_o + n_w], refs[n_o + n_w + 1]
-    outs = refs[n_o + n_w + 2:n_o + n_w + 2 + 2 * n_run]
-    o_scr, w_scr, acc_scr, o_sem, w_sem = refs[n_o + n_w + 2 + 2 * n_run:]
+    outs = refs[n_o + n_w + 2:n_o + n_w + 2 + n_out]
+    o_scr, w_scr, x_scr, acc_scr, o_sem, w_sem, x_sem, out_sem = refs[n_o + n_w + 2 + n_out:]
     width = o_refs[0].shape[1]
     half = width // 2
     n_slots = w_scr.shape[0]
 
     def fetch(k):
-        for i, parts in enumerate(blocks):
+        for i, pieces in enumerate(blocks):
             @pl.when(k == i)
             def _():
-                at = 0
-                for a, r0, n in parts:
-                    pltpu.make_async_copy(w_refs[a].at[pl.ds(r0, n), :], w_scr.at[i % n_slots, pl.ds(at, n), :],
+                to = 0
+                for a, r0, n in pieces:
+                    pltpu.make_async_copy(w_refs[a].at[pl.ds(r0, n), :], w_scr.at[i % n_slots, pl.ds(to, n), :],
                                           w_sem.at[i % n_slots]).start()
-                    at += n
+                    to += n
 
     mine = lax.axis_index('cp')
-    pairs = []
+    loads = [[] for _ in blocks]
     for i in range(n_run):
-        os, rows = o_refs[4 * i:4 * i + 4], pl.ds(i * RUN, RUN)
-        pairs += [(os[0], o_scr.at[rows, pl.ds(0, width)]), (os[1], o_scr.at[rows, pl.ds(width, width)])]
-        for k in range(2, 4):
-            for p, part in enumerate((mine, 1 - mine)):
-                pairs.append((os[k].at[:, pl.ds(pl.multiple_of(part * half, half), half)],
-                              o_scr.at[rows, pl.ds(k * width + p * half, half)]))
-    copies = [pltpu.make_async_copy(src, dst, o_sem.at[i]) for i, (src, dst) in enumerate(pairs)]
-    for cp in copies:
+        rows = pl.ds(i * RUN, RUN)
+        for k in range(4):
+            src = o_refs[4 * i + k]
+            if k < 2:
+                loads[2 * k].append((src, o_scr.at[rows, pl.ds(k * width, width)]))
+            else:
+                for p, part in enumerate((mine, 1 - mine)):
+                    loads[2 * k + p].append((src.at[:, pl.ds(pl.multiple_of(part * half, half), half)],
+                                             o_scr.at[rows, pl.ds(k * width + p * half, half)]))
+    copies = [[pltpu.make_async_copy(src, dst, o_sem.at[k, i]) for i, (src, dst) in enumerate(ls)] for k, ls in enumerate(loads)]
+    x_copy = pltpu.make_async_copy(x_ref.at[pl.ds(at * n_run * RUN, n_run * RUN), :], x_scr, x_sem)
+    for cp in copies[0]:
         cp.start()
     for i in range(n_slots - 1):
         fetch(jnp.int32(i))
+    for ls in copies[1:]:
+        for cp in ls:
+            cp.start()
+    x_copy.start()
     acc_scr[...] = jnp.zeros_like(acc_scr)
-    for cp in copies:
-        cp.wait()
 
     def one(k, carry):
         fetch(k + n_slots - 1)
+        for i, ls in enumerate(copies):
+            if ls:
+                @pl.when(k == i)
+                def _():
+                    for cp in ls:
+                        cp.wait()
         slot = lax.rem(k, n_slots)
         pltpu.make_async_copy(w_scr.at[slot], w_scr.at[slot], w_sem.at[slot]).wait()
         acc_scr[...] += jnp.dot(o_scr[:, pl.ds(pl.multiple_of(k * half, half), half)], w_scr[slot], preferred_element_type=F32)
         return carry
 
     lax.fori_loop(0, len(blocks), one, 0)
-
-    for i in range(n_run):
-        def rows32(r, carry):
-            at = pl.multiple_of(r * 32, 32)
-            rows, mine = pl.ds(at, 32), pl.ds(i * RUN + at, 32)
-            y = (x_ref[mine, :].astype(F32) + acc_scr[mine, :].astype(BF).astype(F32)).astype(BF)
-            outs[2 * i][rows, :] = y
-            outs[2 * i + 1][rows, :] = norm_rows(y, g_ref[...])
-            return carry
-
-        lax.fori_loop(0, RUN // 32, rows32, 0)
-
-
-def out_proj(os, ws, blocks, x_rows, gain, at, after=()):
+    x_copy.wait()
+
+    def rows32(r, carry):
+        rows = pl.ds(pl.multiple_of(r * 32, 32), 32)
+        y = (x_scr[rows, :].astype(F32) + acc_scr[rows, :].astype(BF).astype(F32)).astype(BF)
+        x_scr[rows, :] = y
+        o_scr[rows, :] = norm_rows(y, g_ref[...])
+        return carry
+
+    stores, r0 = [], 0
+    for i, n in enumerate(parts):
+        lax.fori_loop(r0 // 32, (r0 + n) // 32, rows32, 0)
+        for k, scr in enumerate((x_scr, o_scr)):
+            stores.append(pltpu.make_async_copy(scr.at[pl.ds(r0, n), :], outs[2 * i + k], out_sem.at[2 * i + k]))
+            stores[-1].start()
+        r0 += n
+    for cp in stores:
+        cp.wait()
+
+
+def out_proj(os, ws, blocks, x_rows, gain, at, parts, after=()):
     dim = x_rows.shape[1]
     width = os[0].shape[1]
     n_run = len(os) // 4
     rows = n_run * RUN
-    one = lambda m, s: pl.BlockSpec((m, dim), lambda i: (s, 0))
     return pl.pallas_call(
-        ordered(functools.partial(out_kernel, blocks=blocks, n_w=len(ws), n_run=n_run), len(os) + len(ws) + 2, after),
+        ordered(functools.partial(out_kernel, blocks=blocks, n_w=len(ws), n_run=n_run, at=at, parts=parts),
+                len(os) + len(ws) + 2, after),
         grid=(1,),
-        in_specs=[ANY] * (len(os) + len(ws)) + [one(rows, at), pl.BlockSpec((1, dim), lambda i: (0, 0))] + [ANY] * len(after),
-        out_specs=[one(RUN, 0)] * (2 * n_run),
-        out_shape=[jax.ShapeDtypeStruct((RUN, dim), BF)] * (2 * n_run),
-        scratch_shapes=[pltpu.VMEM((rows, 4 * width), BF), pltpu.VMEM((3, width // 2, dim), BF), pltpu.VMEM((rows, dim), F32),
-                        pltpu.SemaphoreType.DMA((6 * n_run,)), pltpu.SemaphoreType.DMA((3,))],
+        in_specs=[ANY] * (len(os) + len(ws) + 1) + [pl.BlockSpec((1, dim), lambda i: (0, 0))] + [ANY] * len(after),
+        out_specs=[ANY] * (2 * len(parts)),
+        out_shape=[jax.ShapeDtypeStruct((n, dim), BF) for n in parts for _ in range(2)],
+        scratch_shapes=[pltpu.VMEM((rows, 4 * width), BF), pltpu.VMEM((3, width // 2, dim), BF), pltpu.VMEM((rows, dim), BF),
+                        pltpu.VMEM((rows, dim), F32), pltpu.SemaphoreType.DMA((len(blocks), 2 * n_run)),
+                        pltpu.SemaphoreType.DMA((3,)), pltpu.SemaphoreType.DMA, pltpu.SemaphoreType.DMA((2 * len(parts),))],
         name="outp", compiler_params=params(1),
-        cost_estimate=pl.CostEstimate(flops=8 * rows * width * dim, transcendentals=0,
-                                      bytes_accessed=8 * width * dim + 8 * rows * dim),
+        cost_estimate=cost(8 * rows * width * dim, 8 * width * dim),
     )(*os, *ws, x_rows, gain, *after)
 
 
-def mlp_kernel(*refs, n_in, tn, nk):
+def mlp_kernel(*refs, n_in, tn, td, nk, nd):
     b_refs = refs[:n_in]
-    wg_ref, wu_ref, wd_ref, keep_ref, send_ref, b_scr, u_scr, sem = refs[n_in:]
+    wg_ref, wu_ref, wd_ref, keep_ref, send_ref, b_scr, u_scr, w_scr, d_scr, b_sem, w_sem, d_sem = refs[n_in:]
     i = pl.program_id(0)
-
-    def gated(rows, cols):
+    rb = b_refs[0].shape[0]
+
+    def fetch(j):
+        @pl.when(j < nk)
+        def _():
+            cols = pl.ds(pl.multiple_of(j * tn, tn), tn)
+            for k, w in enumerate((wg_ref, wu_ref)):
+                pltpu.make_async_copy(w.at[:, cols], w_scr.at[lax.rem(j, 2), k], w_sem.at[lax.rem(j, 2)]).start()
+
+        @pl.when((j >= nk) & (j < nk + nd))
+        def _():
+            n = j - nk
+            pltpu.make_async_copy(wd_ref.at[:, pl.ds(pl.multiple_of(n * td, td), td)], d_scr.at[lax.rem(n, 2)],
+                                  d_sem.at[lax.rem(n, 2)]).start()
+
+    def gated(rows, cols, slot):
         b = b_scr[rows, :]
-        gate = jnp.dot(b, wg_ref[...], preferred_element_type=F32)
-        up = jnp.dot(b, wu_ref[...], preferred_element_type=F32)
+        gate = jnp.dot(b, w_scr[slot, 0], preferred_element_type=F32)
+        up = jnp.dot(b, w_scr[slot, 1], preferred_element_type=F32)
         u_scr[rows, cols] = (jax.nn.silu(gate) * up).astype(BF)
 
     @pl.when(i == 0)
     def _():
-        copies = [pltpu.make_async_copy(r, b_scr.at[pl.ds(k * RUN, RUN), :], sem.at[k]) for k, r in enumerate(b_refs)]
-        for cp in copies:
+        copies = [pltpu.make_async_copy(r, b_scr.at[pl.ds(k * rb, rb), :], b_sem.at[k]) for k, r in enumerate(b_refs)]
+        copies[0].start()
+        fetch(i)
+        for cp in copies[1:]:
             cp.start()
 
+    fetch(i + 1)
+
+    @pl.when(i < nk)
+    def _():
+        pltpu.make_async_copy(w_scr.at[lax.rem(i, 2)], w_scr.at[lax.rem(i, 2)], w_sem.at[lax.rem(i, 2)]).wait()
+
+    @pl.when(i == 0)
+    def _():
         def one(k, carry):
-            rows = pl.ds(pl.multiple_of(k * RUN, RUN), RUN)
-            pltpu.make_async_copy(b_scr.at[rows, :], b_scr.at[rows, :], sem.at[k]).wait()
-            gated(rows, pl.ds(0, tn))
+            rows = pl.ds(pl.multiple_of(k * rb, rb), rb)
+            pltpu.make_async_copy(b_scr.at[rows, :], b_scr.at[rows, :], b_sem.at[k]).wait()
+            gated(rows, pl.ds(0, tn), 0)
             return carry
 
         lax.fori_loop(0, n_in, one, 0)
 
     @pl.when((i > 0) & (i < nk))
     def _():
-        gated(slice(None), pl.ds(pl.multiple_of(i * tn, tn), tn))
+        gated(slice(None), pl.ds(pl.multiple_of(i * tn, tn), tn), lax.rem(i, 2))
 
     @pl.when(i >= nk)
     def _():
-        d = jnp.dot(u_scr[...], wd_ref[...], preferred_element_type=F32).astype(BF)
+        slot = lax.rem(i - nk, 2)
+        pltpu.make_async_copy(d_scr.at[slot], d_scr.at[slot], d_sem.at[slot]).wait()
+        d = jnp.dot(u_scr[...], d_scr[slot], preferred_element_type=F32).astype(BF)
         half = d.shape[0] // 2
         keep_ref[...] = d[:half]
         send_ref[...] = d[half:]
 
 
-def mlp(bs, wg, wu, wd, after=(), tn=256, td=256):
-    rows, dim = RUN * len(bs), bs[0].shape[1]
+def mlp(bs, wg, wu, wd, after=()):
+    rb, dim = bs[0].shape
+    rows = rb * len(bs)
     ffn = wg.shape[1]
+    tn, td = (256, 256) if rows > 512 else (512, 512)
     nk, nd = ffn // tn, dim // td
-    up = lambda i: (0, jnp.minimum(i, nk - 1))
     dn = lambda i: (0, jnp.maximum(i - nk, 0))
     return pl.pallas_call(
-        ordered(functools.partial(mlp_kernel, n_in=len(bs), tn=tn, nk=nk), len(bs) + 3, after),
+        ordered(functools.partial(mlp_kernel, n_in=len(bs), tn=tn, td=td, nk=nk, nd=nd), len(bs) + 3, after),
         grid=(nk + nd,),
-        in_specs=[ANY] * len(bs) + [pl.BlockSpec((dim, tn), up), pl.BlockSpec((dim, tn), up), pl.BlockSpec((ffn, td), dn)]
-        + [ANY] * len(after),
+        in_specs=[ANY] * (len(bs) + 3 + len(after)),
         out_specs=[pl.BlockSpec((rows // 2, td), dn)] * 2,
         out_shape=[jax.ShapeDtypeStruct((rows // 2, dim), BF)] * 2,
-        scratch_shapes=[pltpu.VMEM((rows, dim), BF), pltpu.VMEM((rows, ffn), BF), pltpu.SemaphoreType.DMA((len(bs),))],
+        scratch_shapes=[pltpu.VMEM((rows, dim), BF), pltpu.VMEM((rows, ffn), BF), pltpu.VMEM((2, 2, dim, tn), BF),
+                        pltpu.VMEM((2, ffn, td), BF), pltpu.SemaphoreType.DMA((len(bs),)), pltpu.SemaphoreType.DMA((2,)),
+                        pltpu.SemaphoreType.DMA((2,))],
         name="mlp", compiler_params=params(1),
-        cost_estimate=pl.CostEstimate(flops=6 * rows * dim * ffn, transcendentals=rows * ffn,
-                                      bytes_accessed=6 * dim * ffn + 4 * rows * dim),
+        cost_estimate=cost(6 * rows * dim * ffn, 6 * dim * ffn),
     )(*bs, wg, wu, wd, *after)
 
 
@@ -504,19 +564,18 @@
     z_ref[...] = (y_ref[...].astype(F32) + total.astype(BF).astype(F32)).astype(BF)
 
 
-def sum_run(z, keep, recv, far, y, j, n_runs, after=(), tile=64):
-    dim = y.shape[1]
-    per = RUN // tile
+def sum_rows(z, keep, recv, far, y, first, total, after=(), tile=64):
+    rows, dim = y.shape
     spec = pl.BlockSpec((tile, dim), lambda i: (i, 0))
     prev = () if z is None else (z,)
     return pl.pallas_call(
-        ordered(sum_kernel, len(prev) + 4, after), grid=(per,),
+        ordered(sum_kernel, len(prev) + 4, after), grid=(rows // tile,),
         in_specs=[ANY] * len(prev) + [spec] * 4 + [ANY] * len(after),
-        out_specs=pl.BlockSpec((tile, dim), lambda i: (j * per + i, 0)),
-        out_shape=jax.ShapeDtypeStruct((n_runs * RUN, dim), BF),
+        out_specs=pl.BlockSpec((tile, dim), lambda i: (first // tile + i, 0)),
+        out_shape=jax.ShapeDtypeStruct((total, dim), BF),
         input_output_aliases={0: 0} if prev else {},
         name="zsum", compiler_params=params(1),
-        cost_estimate=pl.CostEstimate(flops=6 * RUN * dim, transcendentals=0, bytes_accessed=10 * RUN * dim),
+        cost_estimate=cost(rows * dim, 8 * rows * dim),
     )(*prev, keep, recv, far, y, *after)
 
 
@@ -637,13 +696,12 @@
             here = tied(far[j], after)
             return [here, send(over_core, here)]
 
-        q_own, kv_own = qkv(own, w_all, (tables, 0))
-        q_mate, kv_mate = qkv(mate, w_all, (tables, n_run), after=(kv_own,))
-        q_a, kv_a = qkv(relayed(0, kv_mate), w_all, (tables, 2 * n_run + 4), after=(kv_mate,))
+        q_here, kv_here = qkv(own + mate, w_all, (tables, 0))
+        q_a, kv_a = qkv(relayed(0, kv_here), w_all, (tables, 2 * n_run + 4), after=(kv_here,))
 
         wo = w_o.reshape(-1, dim)
         half = wo.shape[0] // 2
-        n_piece = 4
+        n_piece = n_run
         rows = half // n_piece
         wo_gated = tied(wo, kv_a)
         wo_x = [send(over_x, lax.dynamic_slice_in_dim(wo_gated, y_id * half + p * rows, rows, axis=0))
@@ -652,12 +710,12 @@
         early = relayed(1, kv_a)
 
         tile = lambda a, n: [(a, i) for i in range(n)]
-        tiles = tile(0, n_run) + tile(1, n_run) + tile(2, 2)
-        st, = flash(tab, [q_own, q_mate, q_a], tiles, [kv_own, kv_mate, kv_a], base=bases[0],
-                   work=int(work[0]), st_tiles=len(tiles))
+        tiles = tile(0, 2 * n_run) + tile(1, 2)
+        st, = flash(tab, [q_here, q_a], tiles, [kv_here, kv_a], base=bases[0], work=int(work[0]),
+                   st_tiles=len(tiles))
         q_b, kv_b = qkv(early + relayed(2, st), w_all, (tables, 2 * n_run), after=(st,))
         q_c, kv_c = qkv(relayed(3, kv_b), w_all, (tables, 2 * n_run + 6), after=(kv_b,))
-        kvs = [kv_own, kv_mate, kv_a, kv_b, kv_c]
+        kvs = [kv_here, kv_a, kv_b, kv_c]
         kvs = kvs + [send(over_y, kv) for kv in kvs]
         q_far = [(q_a, 0), (q_b, 0), (q_b, 2), (q_c, 0)]
 
@@ -678,7 +736,7 @@
             held = 2 * n_run + 2 * j
             carried = [j, n_run + j] + ([held, held + 1] if j == 0 else [None, None])
             o_own, o_mate, o_far, o_fm = flash(
-                tab, [q_own, q_mate, q], [(0, j), (1, j), (2, at), (2, at + 1)], kvs,
+                tab, [q_here, q], [(0, j), (0, n_run + j), (1, at), (1, at + 1)], kvs,
                 base=bases[1 + j], work=int(work[1 + j]), st=st, st_src=carried, after=(prev,))
             os.append([o_own, send(over_core, o_mate), send(over_x, o_far), send(over_both, o_fm)])
             return o_own
@@ -690,25 +748,24 @@
                 for held in (wo_ya, wo_yb):
                     blocks.append([(len(ws) + p, 0, rows) for p in range(n_piece)])
                     ws += [held[p][k] for p in range(n_piece)]
-            got = out_proj(os[2 * i] + os[2 * i + 1], ws, blocks, x_rows, gm, i, after=(prev,))
-            for k in range(2):
-                y, b = got[2 * k:2 * k + 2]
+            parts = (RUN, RUN) if i == 0 else (RUN, RUN // 2, RUN // 2)
+            got = out_proj(os[2 * i] + os[2 * i + 1], ws, blocks, x_rows, gm, i, parts, after=(prev,))
+            for y, b in zip(got[::2], got[1::2]):
                 outs.append((y, b, send(over_x, b), send(over_core, b)))
             return got[0]
 
-        forward_w(0)
-        prev = attend(0)
-        forward_w(1)
-        relay_w(0)
-        prev = attend(1)
-        forward_w(2)
-        forward_w(3)
-        relay_w(1)
-        prev = attend(2)
-        relay_w(2)
-        relay_w(3)
+        last = n_run - 1
+        for j in range(last):
+            forward_w(j)
+            if j:
+                relay_w(j - 1)
+            if j == last - 1:
+                forward_w(last)
+            prev = attend(j)
+        for p in range(last - 1, n_piece):
+            relay_w(p)
         prev = project(0)
-        prev = attend(3)
+        prev = attend(last)
 
         z, sums, relay = None, [], {}
 
@@ -717,24 +774,29 @@
             relay[j] = (here, send(over_core, here))
 
         def finish(j):
-            return sum_run(z, *sums[j], j, n_run, after=() if prev is z else (prev,))
+            first = sum(o[0].shape[0] for o in outs[:j])
+            return sum_rows(z, *sums[j], first, n_run * RUN, after=() if prev is z else (prev,))
 
         relay_b(0)
-        for j in range(n_run):
+        n_part = n_run + 1
+        for j in range(n_part):
             y, b, _, b_mate = outs[j]
             keep, out = mlp([b, relay[j][0], b_mate, relay[j][1]], w_gate, w_up, w_down, after=(prev,))
             recv = send(over_core, out)
             prev = keep
-            if j + 1 < n_run:
-                relay_b(j + 1)
             if j == 0:
+                relay_b(1)
                 prev = project(1)
-            elif j > 1:
-                prev = z = finish(j - 2)
+            else:
+                if j + 1 < n_part:
+                    relay_b(j + 1)
+                if j > 1:
+                    prev = z = finish(j - 2)
             kept = keep if prev is keep else tied(keep, prev)
-            prev = s_far = (kept[RUN:].astype(F32) + recv[RUN:].astype(F32)).astype(BF)
+            half = y.shape[0]
+            prev = s_far = (kept[half:].astype(F32) + recv[half:].astype(F32)).astype(BF)
             sums.append((keep, recv, send(over_x, s_far), y))
-        for j in range(n_run - 2, n_run):
+        for j in (n_part - 2, n_part - 1):
             prev = z = finish(j)
         return z[None]
 

time: 1390 us -> 1290 us (0.928)
  waiting for transfers between devices: 502 us -> 417 us
    ppermute x66 -> x70, waiting for transfers between devices: 502 us -> 417 us  [send(): return lax.ppermute(v, *axis_pairs)]
    ppermute x66 -> x70, starting transfers between devices: 54.9 us -> 48.6 us  [send(): return lax.ppermute(v, *axis_pairs)]
    pallas_call x5 -> x4, Pallas kernels: 96.5 us -> 90.6 us  [qkv(): pl.pallas_call(ordered(functools.partial(qkv_kernel, n_in=n_in, n_q=n_q,...]
    pallas_call x4 -> x5, Pallas kernels: 361 us -> 362 us  [mlp(): pl.pallas_call(ordered(functools.partial(mlp_kernel, n_in=len(bs), tn=tn,...]
  transfers between devices with their start and end apart: 66 -> 70, of which waited for: 30 -> 30; matrix products, arithmetic and copies ran while one was open for 3% -> 4% of each run, Pallas kernels for 34% -> 43%
where the time goes in v6:
time: 1290 us; the launch traced here: 1280 us
  Pallas kernels  762 us (59%)
  waiting for transfers between devices  417 us (32%)
  starting transfers between devices  48.6 us (4%)
  other arithmetic  24.5 us (2%)
  local copies, waits for them, and re-layouts  23.6 us (2%)
    ppermute x70, waiting for transfers between devices, send(): return lax.ppermute(v, *axis_pairs)  417 us
    pallas_call x5, Pallas kernels, mlp(): pl.pallas_call(ordered(functools.partial(mlp_kernel, n_in=len(bs), tn=tn,...  362 us
    pallas_call x5, Pallas kernels, flash(): pl.pallas_call(ordered(functools.partial(flash_kernel, q_src=q_src, kv_sr...  215 us
    pallas_call x4, Pallas kernels, qkv(): pl.pallas_call(ordered(functools.partial(qkv_kernel, n_in=n_in, n_q=n_q,...  90.6 us
    pallas_call x2, Pallas kernels, out_proj(): pl.pallas_call(ordered(functools.partial(out_kernel, blocks=blocks, n_w=l...  57.7 us
    ppermute x70, starting transfers between devices, send(): return lax.ppermute(v, *axis_pairs)  48.6 us
  transfers between devices with their start and end apart: 70, of which 30 were waited for; matrix products, arithmetic and copies ran while one was open for 4% of the time, Pallas kernels for 43%

profile of v6, /device:TPU:0, one launch (start us, length us, event | category | flops | bytes accessed | tf_op | source)
XLA Modules:
  0.0 1276.9 jit_solution(4953456367296407500)
XLA Ops:
  20.0 9.4 bitcast_dynamic-update-slice_fusion
  29.4 4.8 multiply_sine_fusion
  38.3 39.7 %qkv.4 = (bf16[8,1024,256]{2,1,0:T(8,128)(2,1)}, bf16[8,2,256,256]{3,2,1,0:T(8,128)(2,1)}) custom-call(bf16[256,4096]{1,0:T(8,128)(2,1)} %norm.4.refs_2_.refs_0_, bf16[256,4096]{1,0:T(8,128)(2,1)} %norm.5.refs_2_.refs_1_, bf16[256,4096]{1,0:T(8,128)(2,1)} %norm.6.refs_2_, bf16[256,4096]{1,0:T(8,128)(2,1)} %norm.7.refs_3_, ...), custom_call_target="tpu_custom_call" | custom-call | flops 25769803776 | bytes 12582912 | tf_op jit(solution)/shard_map/qkv/pallas_call | solution.py:124
  82.5 14.1 %qkv.5 = (bf16[2,1024,256]{2,1,0:T(8,128)(2,1)}, bf16[2,2,256,256]{3,2,1,0:T(8,128)(2,1)}) custom-call(bf16[256,4096]{1,0:T(8,128)(2,1)} %collective-permute-done.4.refs_0_, bf16[256,4096]{1,0:T(8,128)(2,1)} %collective-permute-done.5.refs_1_, bf16[4096,1536]{1,0:T(8,128)(2,1)} %bitcast_dynamic-update-slice_fusion.1.refs_8_.refs_2_.refs_4_, ...), custom_call_target="tpu_custom_call" | custom-call | flops 6442450944 | bytes 12582912 | tf_op jit(solution)/shard_map/qkv/pallas_call | solution.py:124
  96.7 30.2 %collective-permute-done.6.refs_0_ = bf16[256,4096]{1,0:T(8,128)(2,1)} collective-permute-done((bf16[256,4096]{1,0:T(8,128)(2,1)}, bf16[256,4096]{1,0:T(8,128)(2,1)}, u32[]{:S(2)}, u32[]{:S(2)}) %collective-permute-start.6) | collective-permute-done | bytes 2097184 | tf_op jit(solution)/shard_map/ppermute | solution.py:683
  126.9 53.1 %flash_part.1.refs_7_.refs_11_ = f32[10,2,4,144,256]{4,3,2,1,0:T(8,128)} custom-call(s32[969]{0:T(1024)} %bitcast.28, bf16[8,1024,256]{2,1,0:T(8,128)(2,1)} %get-tuple-element.79.refs_1_, bf16[2,1024,256]{2,1,0:T(8,128)(2,1)} %get-tuple-element.82.refs_2_, bf16[8,2,256,256]{3,2,1,0:T(8,128)(2,1)} %get-tuple-element.80.refs_5_.refs_3_, ...), custom_call_target="tpu_custom_call" | custom-call | flops 38654705664 | bytes 2621440 | tf_op jit(solution)/shard_map/flash_part/pallas_call | solution.py:351
  186.3 22.6 %qkv.6 = (bf16[4,1024,256]{2,1,0:T(8,128)(2,1)}, bf16[4,2,256,256]{3,2,1,0:T(8,128)(2,1)}) custom-call(bf16[256,4096]{1,0:T(8,128)(2,1)} %collective-permute-done.6.refs_0_, bf16[256,4096]{1,0:T(8,128)(2,1)} %collective-permute-done.7.refs_1_, bf16[256,4096]{1,0:T(8,128)(2,1)} %collective-permute-done.8.refs_2_, ...), custom_call_target="tpu_custom_call" | custom-call | flops 12884901888 | bytes 12582912 | tf_op jit(solution)/shard_map/qkv/pallas_call | solution.py:124
  208.9 21.1 %collective-permute-done.10.refs_0_ = bf16[256,4096]{1,0:T(8,128)(2,1)} collective-permute-done((bf16[256,4096]{1,0:T(8,128)(2,1)}, bf16[256,4096]{1,0:T(8,128)(2,1)}, u32[]{:S(2)}, u32[]{:S(2)}) %collective-permute-start.10) | collective-permute-done | bytes 2097184 | tf_op jit(solution)/shard_map/ppermute | solution.py:683
  232.1 4.2 constant_dynamic-slice_fusion
  238.8 14.1 %qkv.7 = (bf16[2,1024,256]{2,1,0:T(8,128)(2,1)}, bf16[2,2,256,256]{3,2,1,0:T(8,128)(2,1)}) custom-call(bf16[256,4096]{1,0:T(8,128)(2,1)} %collective-permute-done.10.refs_0_, bf16[256,4096]{1,0:T(8,128)(2,1)} %collective-permute-done.11.refs_1_, bf16[4096,1536]{1,0:T(8,128)(2,1)} %bitcast_dynamic-update-slice_fusion.1.refs_8_.refs_2_.refs_4_, ...), custom_call_target="tpu_custom_call" | custom-call | flops 6442450944 | bytes 12582912 | tf_op jit(solution)/shard_map/qkv/pallas_call | solution.py:124
  252.9 8.7 collective-permute-done.23.refs_10_
  261.6 17.2 %collective-permute-done.12.refs_7_ = bf16[8,2,256,256]{3,2,1,0:T(8,128)(2,1)} collective-permute-done((bf16[8,2,256,256]{3,2,1,0:T(8,128)(2,1)}, bf16[8,2,256,256]{3,2,1,0:T(8,128)(2,1)}, u32[]{:S(2)}, u32[]{:S(2)}) %collective-permute-start.12) | collective-permute-done | bytes 2097184 | tf_op jit(solution)/shard_map/ppermute | solution.py:683
  279.3 10.8 collective-permute-done.13.refs_8_
  290.5 22.0 %collective-permute-done.14.refs_9_ = bf16[4,2,256,256]{3,2,1,0:T(8,128)(2,1)} collective-permute-done((bf16[4,2,256,256]{3,2,1,0:T(8,128)(2,1)}, bf16[4,2,256,256]{3,2,1,0:T(8,128)(2,1)}, u32[]{:S(2)}, u32[]{:S(2)}) %collective-permute-start.14) | collective-permute-done | bytes 1048608 | tf_op jit(solution)/shard_map/ppermute | solution.py:683
  313.0 10.3 collective-permute-done.15.refs_10_
  323.3 29.3 %flash.4 = (bf16[256,1024]{1,0:T(8,128)(2,1)}, bf16[256,1024]{1,0:T(8,128)(2,1)}, bf16[256,1024]{1,0:T(8,128)(2,1)}, bf16[256,1024]{1,0:T(8,128)(2,1)}) custom-call(s32[969]{0:T(1024)} %bitcast.29, bf16[8,1024,256]{2,1,0:T(8,128)(2,1)} %get-tuple-element.79.refs_1_, bf16[2,1024,256]{2,1,0:T(8,128)(2,1)} %get-tuple-element.82.refs_2_, ...), custom_call_target="tpu_custom_call" | custom-call | flops 27917287424 | bytes 8388608 | tf_op jit(solution)/shard_map/flash/pallas_call | solution.py:351
  353.7 11.9 collective-permute-start.17
  365.6 44.6 %flash.5 = (bf16[256,1024]{1,0:T(8,128)(2,1)}, bf16[256,1024]{1,0:T(8,128)(2,1)}, bf16[256,1024]{1,0:T(8,128)(2,1)}, bf16[256,1024]{1,0:T(8,128)(2,1)}) custom-call(s32[969]{0:T(1024)} %bitcast.30, bf16[8,1024,256]{2,1,0:T(8,128)(2,1)} %get-tuple-element.79.refs_1_, bf16[4,1024,256]{2,1,0:T(8,128)(2,1)} %get-tuple-element.93.refs_2_, ...), custom_call_target="tpu_custom_call" | custom-call | flops 32212254720 | bytes 8388608 | tf_op jit(solution)/shard_map/flash/pallas_call | solution.py:351
  416.1 11.6 collective-permute-done.20.refs_6_
  427.7 9.1 collective-permute-done.28.refs_15_
  436.8 22.5 %collective-permute-done.29.refs_16_ = bf16[128,4096]{1,0:T(8,128)(2,1)} collective-permute-done((bf16[128,4096]{1,0:T(8,128)(2,1)}, bf16[128,4096]{1,0:T(8,128)(2,1)}, u32[]{:S(2)}, u32[]{:S(2)}) %collective-permute-start.29) | collective-permute-done | bytes 1048608 | tf_op jit(solution)/shard_map/ppermute | solution.py:683
  459.2 21.9 %collective-permute-done.30.refs_17_ = bf16[128,4096]{1,0:T(8,128)(2,1)} collective-permute-done((bf16[128,4096]{1,0:T(8,128)(2,1)}, bf16[128,4096]{1,0:T(8,128)(2,1)}, u32[]{:S(2)}, u32[]{:S(2)}) %collective-permute-start.30) | collective-permute-done | bytes 1048608 | tf_op jit(solution)/shard_map/ppermute | solution.py:683
  481.5 44.5 %flash.6 = (bf16[256,1024]{1,0:T(8,128)(2,1)}, bf16[256,1024]{1,0:T(8,128)(2,1)}, bf16[256,1024]{1,0:T(8,128)(2,1)}, bf16[256,1024]{1,0:T(8,128)(2,1)}) custom-call(s32[969]{0:T(1024)} %bitcast.31, bf16[8,1024,256]{2,1,0:T(8,128)(2,1)} %get-tuple-element.79.refs_1_, bf16[4,1024,256]{2,1,0:T(8,128)(2,1)} %get-tuple-element.93.refs_2_, ...), custom_call_target="tpu_custom_call" | custom-call | flops 32212254720 | bytes 8388608 | tf_op jit(solution)/shard_map/flash/pallas_call | solution.py:351
  534.5 29.1 %outp.2 = (bf16[256,4096]{1,0:T(8,128)(2,1)}, bf16[256,4096]{1,0:T(8,128)(2,1)}, bf16[256,4096]{1,0:T(8,128)(2,1)}, bf16[256,4096]{1,0:T(8,128)(2,1)}) custom-call(bf16[256,1024]{1,0:T(8,128)(2,1)} %get-tuple-element.89.refs_12_.refs_0_, bf16[256,1024]{1,0:T(8,128)(2,1)} %collective-permute-done.16.refs_1_, ...), custom_call_target="tpu_custom_call" | custom-call | flops 17179869184 | bytes 33554432 | tf_op jit(solution)/shard_map/outp/pallas_call | solution.py:462
  564.5 43.8 %flash.7 = (bf16[256,1024]{1,0:T(8,128)(2,1)}, bf16[256,1024]{1,0:T(8,128)(2,1)}, bf16[256,1024]{1,0:T(8,128)(2,1)}, bf16[256,1024]{1,0:T(8,128)(2,1)}) custom-call(s32[969]{0:T(1024)} %bitcast.32, bf16[8,1024,256]{2,1,0:T(8,128)(2,1)} %get-tuple-element.79.refs_1_, bf16[2,1024,256]{2,1,0:T(8,128)(2,1)} %get-tuple-element.109.refs_2_, ...), custom_call_target="tpu_custom_call" | custom-call | flops 32212254720 | bytes 8388608 | tf_op jit(solution)/shard_map/flash/pallas_call | solution.py:351
  616.6 88.4 %mlp.5 = (bf16[512,4096]{1,0:T(8,128)(2,1)}, bf16[512,4096]{1,0:T(8,128)(2,1)}) custom-call(bf16[256,4096]{1,0:T(8,128)(2,1)} %get-tuple-element.108.refs_0_, bf16[256,4096]{1,0:T(8,128)(2,1)} %collective-permute-done.39.refs_1_, bf16[256,4096]{1,0:T(8,128)(2,1)} %collective-permute-done.40.refs_2_, bf16[256,4096]{1,0:T(8,128)(2,1)} %collective-permute-done.41.refs_3_, ...), custom_call_target="tpu_custom_call" | custom-call | flops 77309411328 | bytes 75497472 | tf_op jit(solution)/shard_map/mlp/pallas_call | solution.py:547
  707.0 6.2 collective-permute-done.43.refs_1_
  713.4 7.2 collective-permute-done.44.refs_2_
  721.1 9.1 collective-permute-done.45.refs_3_
  731.7 11.4 collective-permute-done.47.refs_6_
  743.1 9.6 collective-permute-done.48.refs_7_
  752.6 28.6 %outp.3 = (bf16[256,4096]{1,0:T(8,128)(2,1)}, bf16[256,4096]{1,0:T(8,128)(2,1)}, bf16[128,4096]{1,0:T(8,128)(2,1)}, bf16[128,4096]{1,0:T(8,128)(2,1)}, bf16[128,...) custom-call(bf16[256,1024]{1,0:T(8,128)(2,1)} %get-tuple-element.105.refs_28_.refs_0_, ...), custom_call_target="tpu_custom_call" | custom-call | flops 17179869184 | bytes 33554432 | tf_op jit(solution)/shard_map/outp/pallas_call | solution.py:462
  781.2 4.3 add_convert_fusion.2.refs_7_
  785.5 88.6 %mlp.6 = (bf16[512,4096]{1,0:T(8,128)(2,1)}, bf16[512,4096]{1,0:T(8,128)(2,1)}) custom-call(bf16[256,4096]{1,0:T(8,128)(2,1)} %get-tuple-element.124.refs_0_, bf16[256,4096]{1,0:T(8,128)(2,1)} %collective-permute-done.51.refs_1_, bf16[256,4096]{1,0:T(8,128)(2,1)} %collective-permute-done.52.refs_2_, bf16[256,4096]{1,0:T(8,128)(2,1)} %collective-permute-done.53.refs_3_, ...), custom_call_target="tpu_custom_call" | custom-call | flops 77309411328 | bytes 75497472 | tf_op jit(solution)/shard_map/mlp/pallas_call | solution.py:547
  875.3 47.3 %collective-permute-done.50.refs_1_ = bf16[256,4096]{1,0:T(8,128)(2,1)S(1)} collective-permute-done((bf16[256,4096]{1,0:T(8,128)(2,1)}, bf16[256,4096]{1,0:T(8,128)(2,1)S(1)}, u32[]{:S(2)}, u32[]{:S(2)}) %collective-permute-start.50) | collective-permute-done | bytes 2097184 | tf_op jit(solution)/shard_map/ppermute | solution.py:683
  922.6 5.3 add_convert_fusion.1.refs_7_
  929.3 88.5 %mlp.7 = (bf16[512,4096]{1,0:T(8,128)(2,1)}, bf16[512,4096]{1,0:T(8,128)(2,1)}) custom-call(bf16[256,4096]{1,0:T(8,128)(2,1)} %get-tuple-element.123.refs_0_, bf16[256,4096]{1,0:T(8,128)(2,1)} %copy-done.3, bf16[256,4096]{1,0:T(8,128)(2,1)} %copy-done.4, bf16[256,4096]{1,0:T(8,128)(2,1)} %collective-permute-done.55.refs_3_, bf16[4096,3072]{1,0:T(8,128)(2,1)} %refs_4_.9, ...), custom_call_target="tpu_custom_call" | custom-call | flops 77309411328 | bytes 75497472 | tf_op jit(solution)/shard_map/mlp/pallas_call | solution.py:547
  1020.7 46.4 %collective-permute-done.49.refs_2_ = bf16[256,4096]{1,0:T(8,128)(2,1)} collective-permute-done((bf16[256,4096]{1,0:T(8,128)(2,1)}, bf16[256,4096]{1,0:T(8,128)(2,1)}, u32[]{:S(2)}, u32[]{:S(2)}) %collective-permute-start.49) | collective-permute-done | bytes 2097184 | tf_op jit(solution)/shard_map/ppermute | solution.py:683
  1067.0 5.6 zsum.5.refs_0_
  1072.6 16.9 %collective-permute-done.58.refs_1_ = bf16[128,4096]{1,0:T(8,128)(2,1)} collective-permute-done((bf16[128,4096]{1,0:T(8,128)(2,1)}, bf16[128,4096]{1,0:T(8,128)(2,1)}, u32[]{:S(2)}, u32[]{:S(2)}) %collective-permute-start.58) | collective-permute-done | bytes 1048608 | tf_op jit(solution)/shard_map/ppermute | solution.py:683
  1089.5 4.4 add_convert_fusion.refs_7_
  1093.9 48.2 %mlp.8 = (bf16[256,4096]{1,0:T(8,128)(2,1)}, bf16[256,4096]{1,0:T(8,128)(2,1)}) custom-call(bf16[128,4096]{1,0:T(8,128)(2,1)} %get-tuple-element.131.refs_0_, bf16[128,4096]{1,0:T(8,128)(2,1)} %collective-permute-done.58.refs_1_, bf16[128,4096]{1,0:T(8,128)(2,1)} %collective-permute-done.59.refs_2_, bf16[128,4096]{1,0:T(8,128)(2,1)} %collective-permute-done.60.refs_3_, ...), custom_call_target="tpu_custom_call" | custom-call | flops 38654705664 | bytes 75497472 | tf_op jit(solution)/shard_map/mlp/pallas_call | solution.py:547
  1143.0 25.0 %collective-permute-done.63.refs_1_ = bf16[128,4096]{1,0:T(8,128)(2,1)} collective-permute-done((bf16[128,4096]{1,0:T(8,128)(2,1)}, bf16[128,4096]{1,0:T(8,128)(2,1)}, u32[]{:S(2)}, u32[]{:S(2)}) %collective-permute-start.63) | collective-permute-done | bytes 1048608 | tf_op jit(solution)/shard_map/ppermute | solution.py:683
  1168.5 5.6 zsum.6.refs_0_
  1176.8 48.0 %mlp.9 = (bf16[256,4096]{1,0:T(8,128)(2,1)}, bf16[256,4096]{1,0:T(8,128)(2,1)}) custom-call(bf16[128,4096]{1,0:T(8,128)(2,1)} %get-tuple-element.136.refs_0_, bf16[128,4096]{1,0:T(8,128)(2,1)} %collective-permute-done.63.refs_1_, bf16[128,4096]{1,0:T(8,128)(2,1)} %collective-permute-done.64.refs_2_, bf16[128,4096]{1,0:T(8,128)(2,1)} %collective-permute-done.65.refs_3_, ...), custom_call_target="tpu_custom_call" | custom-call | flops 38654705664 | bytes 75497472 | tf_op jit(solution)/shard_map/mlp/pallas_call | solution.py:547
  1226.6 5.6 zsum.7.refs_0_
  1235.5 15.9 %collective-permute-done.67.refs_3_ = bf16[128,4096]{1,0:T(8,128)(2,1)} collective-permute-done((bf16[128,4096]{1,0:T(8,128)(2,1)}, bf16[128,4096]{1,0:T(8,128)(2,1)}, u32[]{:S(2)}, u32[]{:S(2)}) %collective-permute-start.67) | collective-permute-done | bytes 1048608 | tf_op jit(solution)/shard_map/ppermute | solution.py:683
  1254.6 18.5 %collective-permute-done.69.refs_3_ = bf16[128,4096]{1,0:T(8,128)(2,1)} collective-permute-done((bf16[128,4096]{1,0:T(8,128)(2,1)}, bf16[128,4096]{1,0:T(8,128)(2,1)}, u32[]{:S(2)}, u32[]{:S(2)}) %collective-permute-start.69) | collective-permute-done | bytes 1048608 | tf_op jit(solution)/shard_map/ppermute | solution.py:683
  (143 shorter events, 90.7 us)
Async XLA Ops:
  4.7 73.3 %collective-permute-start.4 = (bf16[256,4096]{1,0:T(8,128)(2,1)}, bf16[256,4096]{1,0:T(8,128)(2,1)}, u32[]{:S(2)}, u32[]{:S(2)}) collective-permute-start(bf16[256,4096]{1,0:T(8,128)(2,1)} %norm.4.refs_2_.refs_0_), channel_id=1, source_target_pairs={{0,2},{1,3},{2,0},{3,1},{4,6},{5,7},{6,4},{7,5}} | collective-permute-start | bytes 6291464 | tf_op jit(solution)/shard_map/ppermute | solution.py:683
  8.0 30.2 %collective-permute-start = (bf16[256,4096]{1,0:T(8,128)(2,1)}, bf16[256,4096]{1,0:T(8,128)(2,1)}, u32[]{:S(2)}, u32[]{:S(2)}) collective-permute-start(bf16[256,4096]{1,0:T(8,128)(2,1)} %norm.4.refs_2_.refs_0_), channel_id=1, source_target_pairs={{0,1},{1,0},{2,3},{3,2},{4,5},{5,4},{6,7},{7,6}} | collective-permute-start | bytes 6291464 | tf_op jit(solution)/shard_map/ppermute | solution.py:683
  11.4 26.8 %collective-permute-start.1 = (bf16[256,4096]{1,0:T(8,128)(2,1)}, bf16[256,4096]{1,0:T(8,128)(2,1)}, u32[]{:S(2)}, u32[]{:S(2)}) collective-permute-start(bf16[256,4096]{1,0:T(8,128)(2,1)} %norm.5.refs_2_.refs_1_), channel_id=1, source_target_pairs={{0,1},{1,0},{2,3},{3,2},{4,5},{5,4},{6,7},{7,6}} | collective-permute-start | bytes 6291464 | tf_op jit(solution)/shard_map/ppermute | solution.py:683
  78.0 48.8 %collective-permute-start.6 = (bf16[256,4096]{1,0:T(8,128)(2,1)}, bf16[256,4096]{1,0:T(8,128)(2,1)}, u32[]{:S(2)}, u32[]{:S(2)}) collective-permute-start(bf16[256,4096]{1,0:T(8,128)(2,1)} %norm.5.refs_2_.refs_1_), channel_id=1, source_target_pairs={{0,2},{1,3},{2,0},{3,1},{4,6},{5,7},{6,4},{7,5}} | collective-permute-start | bytes 6291464 | tf_op jit(solution)/shard_map/ppermute | solution.py:683
  78.1 101.9 %collective-permute-start.8 = (bf16[256,4096]{1,0:T(8,128)(2,1)}, bf16[256,4096]{1,0:T(8,128)(2,1)}, u32[]{:S(2)}, u32[]{:S(2)}) collective-permute-start(bf16[256,4096]{1,0:T(8,128)(2,1)} %norm.6.refs_2_), channel_id=1, source_target_pairs={{0,2},{1,3},{2,0},{3,1},{4,6},{5,7},{6,4},{7,5}} | collective-permute-start | bytes 6291464 | tf_op jit(solution)/shard_map/ppermute | solution.py:683
  126.9 55.3 %collective-permute-start.7 = (bf16[256,4096]{1,0:T(8,128)(2,1)}, bf16[256,4096]{1,0:T(8,128)(2,1)}, u32[]{:S(2)}, u32[]{:S(2)}) collective-permute-start(bf16[256,4096]{1,0:T(8,128)(2,1)} %collective-permute-done.6.refs_0_), channel_id=1, source_target_pairs={{0,1},{1,0},{2,3},{3,2},{4,5},{5,4},{6,7},{7,6}} | collective-permute-start | bytes 6291464 | tf_op jit(solution)/shard_map/ppermute | solution.py:683
  182.1 47.9 %collective-permute-start.10 = (bf16[256,4096]{1,0:T(8,128)(2,1)}, bf16[256,4096]{1,0:T(8,128)(2,1)}, u32[]{:S(2)}, u32[]{:S(2)}) collective-permute-start(bf16[256,4096]{1,0:T(8,128)(2,1)} %norm.7.refs_3_), channel_id=1, source_target_pairs={{0,2},{1,3},{2,0},{3,1},{4,6},{5,7},{6,4},{7,5}} | collective-permute-start | bytes 6291464 | tf_op jit(solution)/shard_map/ppermute | solution.py:683
  230.0 48.8 %collective-permute-start.12 = (bf16[8,2,256,256]{3,2,1,0:T(8,128)(2,1)}, bf16[8,2,256,256]{3,2,1,0:T(8,128)(2,1)}, u32[]{:S(2)}, u32[]{:S(2)}) collective-permute-start(bf16[8,2,256,256]{3,2,1,0:T(8,128)(2,1)} %get-tuple-element.80.refs_5_.refs_3_), channel_id=1, source_target_pairs={{0,4},{4,0},{1,5},{5,1},{2,6},{6,2},{3,7},{7,3}} | collective-permute-start | bytes 6291464 | tf_op jit(solution)/shard_map/ppermute | solution.py:683
  231.6 58.5 %collective-permute-start.13 = (bf16[2,2,256,256]{3,2,1,0:T(8,128)(2,1)}, bf16[2,2,256,256]{3,2,1,0:T(8,128)(2,1)}, u32[]{:S(2)}, u32[]{:S(2)}) collective-permute-start(bf16[2,2,256,256]{3,2,1,0:T(8,128)(2,1)} %get-tuple-element.83.refs_4_), channel_id=1, source_target_pairs={{0,4},{4,0},{1,5},{5,1},{2,6},{6,2},{3,7},{7,3}} | collective-permute-start | bytes 1572872 | tf_op jit(solution)/shard_map/ppermute | solution.py:683
  236.8 75.8 %collective-permute-start.14 = (bf16[4,2,256,256]{3,2,1,0:T(8,128)(2,1)}, bf16[4,2,256,256]{3,2,1,0:T(8,128)(2,1)}, u32[]{:S(2)}, u32[]{:S(2)}) collective-permute-start(bf16[4,2,256,256]{3,2,1,0:T(8,128)(2,1)} %get-tuple-element.86.refs_5_), channel_id=1, source_target_pairs={{0,4},{4,0},{1,5},{5,1},{2,6},{6,2},{3,7},{7,3}} | collective-permute-start | bytes 3145736 | tf_op jit(solution)/shard_map/ppermute | solution.py:683
  252.9 70.5 %collective-permute-start.15 = (bf16[2,2,256,256]{3,2,1,0:T(8,128)(2,1)}, bf16[2,2,256,256]{3,2,1,0:T(8,128)(2,1)}, u32[]{:S(2)}, u32[]{:S(2)}) collective-permute-start(bf16[2,2,256,256]{3,2,1,0:T(8,128)(2,1)} %get-tuple-element.88.refs_6_.refs_12_), channel_id=1, source_target_pairs={{0,4},{4,0},{1,5},{5,1},{2,6},{6,2},{3,7},{7,3}} | collective-permute-start | bytes 1572872 | tf_op jit(solution)/shard_map/ppermute | solution.py:683
  261.6 272.9 %collective-permute-start.22 = (bf16[1024,4096]{1,0:T(8,128)(2,1)}, bf16[1024,4096]{1,0:T(8,128)(2,1)}, u32[]{:S(2)}, u32[]{:S(2)}) collective-permute-start(bf16[1024,4096]{1,0:T(8,128)(2,1)} %bitcast.23), channel_id=1, source_target_pairs={{0,1},{1,0},{2,3},{3,2},{4,5},{5,4},{6,7},{7,6}} | collective-permute-start | bytes 25165832 | tf_op jit(solution)/shard_map/ppermute | solution.py:683
  278.9 73.8 %collective-permute-start.26 = (bf16[128,4096]{1,0:T(8,128)(2,1)}, bf16[128,4096]{1,0:T(8,128)(2,1)}, u32[]{:S(2)}, u32[]{:S(2)}) collective-permute-start(bf16[128,4096]{1,0:T(8,128)(2,1)} %get-tuple-element.145), channel_id=1, source_target_pairs={{0,2},{1,3},{2,0},{3,1},{4,6},{5,7},{6,4},{7,5}} | collective-permute-start | bytes 3145736 | tf_op jit(solution)/shard_map/ppermute | solution.py:683
  290.1 63.4 %collective-permute-start.25 = (bf16[128,4096]{1,0:T(8,128)(2,1)}, bf16[128,4096]{1,0:T(8,128)(2,1)}, u32[]{:S(2)}, u32[]{:S(2)}) collective-permute-start(bf16[128,4096]{1,0:T(8,128)(2,1)} %get-tuple-element.146), channel_id=1, source_target_pairs={{0,2},{1,3},{2,0},{3,1},{4,6},{5,7},{6,4},{7,5}} | collective-permute-start | bytes 3145736 | tf_op jit(solution)/shard_map/ppermute | solution.py:683
  312.6 41.2 %collective-permute-start.24 = (bf16[128,4096]{1,0:T(8,128)(2,1)}, bf16[128,4096]{1,0:T(8,128)(2,1)}, u32[]{:S(2)}, u32[]{:S(2)}) collective-permute-start(bf16[128,4096]{1,0:T(8,128)(2,1)} %get-tuple-element.147), channel_id=1, source_target_pairs={{0,2},{1,3},{2,0},{3,1},{4,6},{5,7},{6,4},{7,5}} | collective-permute-start | bytes 3145736 | tf_op jit(solution)/shard_map/ppermute | solution.py:683
  323.3 42.3 %collective-permute-start.31 = (bf16[128,4096]{1,0:T(8,128)(2,1)}, bf16[128,4096]{1,0:T(8,128)(2,1)}, u32[]{:S(2)}, u32[]{:S(2)}) collective-permute-start(bf16[128,4096]{1,0:T(8,128)(2,1)} %collective-permute-done.23.refs_10_), channel_id=1, source_target_pairs={{0,1},{1,0},{2,3},{3,2},{4,5},{5,4},{6,7},{7,6}} | collective-permute-start | bytes 3145736 | tf_op jit(solution)/shard_map/ppermute | solution.py:683
  352.7 57.6 %collective-permute-start.27 = (bf16[128,4096]{1,0:T(8,128)(2,1)}, bf16[128,4096]{1,0:T(8,128)(2,1)}, u32[]{:S(2)}, u32[]{:S(2)}) collective-permute-start(bf16[128,4096]{1,0:T(8,128)(2,1)} %collective-permute-done.23.refs_10_), channel_id=1, source_target_pairs={{0,4},{4,0},{1,5},{5,1},{2,6},{6,2},{3,7},{7,3}} | collective-permute-start | bytes 3145736 | tf_op jit(solution)/shard_map/ppermute | solution.py:683
  353.5 56.9 %collective-permute-start.16 = (bf16[256,1024]{1,0:T(8,128)(2,1)}, bf16[256,1024]{1,0:T(8,128)(2,1)}, u32[]{:S(2)}, u32[]{:S(2)}) collective-permute-start(bf16[256,1024]{1,0:T(8,128)(2,1)} %get-tuple-element.90), channel_id=1, source_target_pairs={{0,1},{1,0},{2,3},{3,2},{4,5},{5,4},{6,7},{7,6}} | collective-permute-start | bytes 1572872 | tf_op jit(solution)/shard_map/ppermute | solution.py:683
  353.7 57.3 %collective-permute-start.17 = (bf16[256,1024]{1,0:T(8,128)(2,1)}, bf16[256,1024]{1,0:T(8,128)(2,1)}, u32[]{:S(2)}, u32[]{:S(2)}) collective-permute-start(bf16[256,1024]{1,0:T(8,128)(2,1)} %get-tuple-element.91), channel_id=1, source_target_pairs={{0,2},{1,3},{2,0},{3,1},{4,6},{5,7},{6,4},{7,5}} | collective-permute-start | bytes 1572872 | tf_op jit(solution)/shard_map/ppermute | solution.py:683
  365.6 46.8 %collective-permute-start.18 = (bf16[256,1024]{1,0:T(8,128)(2,1)}, bf16[256,1024]{1,0:T(8,128)(2,1)}, u32[]{:S(2)}, u32[]{:S(2)}) collective-permute-start(bf16[256,1024]{1,0:T(8,128)(2,1)} %get-tuple-element.92), channel_id=1, source_target_pairs={{0,3},{1,2},{2,1},{3,0},{4,7},{5,6},{6,5},{7,4}} | collective-permute-start | bytes 1572872 | tf_op jit(solution)/shard_map/ppermute | solution.py:683
  410.4 26.3 %collective-permute-start.28 = (bf16[128,4096]{1,0:T(8,128)(2,1)}, bf16[128,4096]{1,0:T(8,128)(2,1)}, u32[]{:S(2)}, u32[]{:S(2)}) collective-permute-start(bf16[128,4096]{1,0:T(8,128)(2,1)} %collective-permute-done.24.refs_11_), channel_id=1, source_target_pairs={{0,4},{4,0},{1,5},{5,1},{2,6},{6,2},{3,7},{7,3}} | collective-permute-start | bytes 3145736 | tf_op jit(solution)/shard_map/ppermute | solution.py:683
  411.0 48.2 %collective-permute-start.29 = (bf16[128,4096]{1,0:T(8,128)(2,1)}, bf16[128,4096]{1,0:T(8,128)(2,1)}, u32[]{:S(2)}, u32[]{:S(2)}) collective-permute-start(bf16[128,4096]{1,0:T(8,128)(2,1)} %collective-permute-done.25.refs_12_), channel_id=1, source_target_pairs={{0,4},{4,0},{1,5},{5,1},{2,6},{6,2},{3,7},{7,3}} | collective-permute-start | bytes 3145736 | tf_op jit(solution)/shard_map/ppermute | solution.py:683
  412.4 68.7 %collective-permute-start.30 = (bf16[128,4096]{1,0:T(8,128)(2,1)}, bf16[128,4096]{1,0:T(8,128)(2,1)}, u32[]{:S(2)}, u32[]{:S(2)}) collective-permute-start(bf16[128,4096]{1,0:T(8,128)(2,1)} %collective-permute-done.26.refs_13_), channel_id=1, source_target_pairs={{0,4},{4,0},{1,5},{5,1},{2,6},{6,2},{3,7},{7,3}} | collective-permute-start | bytes 3145736 | tf_op jit(solution)/shard_map/ppermute | solution.py:683
  427.7 99.7 %collective-permute-start.32 = (bf16[128,4096]{1,0:T(8,128)(2,1)}, bf16[128,4096]{1,0:T(8,128)(2,1)}, u32[]{:S(2)}, u32[]{:S(2)}) collective-permute-start(bf16[128,4096]{1,0:T(8,128)(2,1)} %collective-permute-done.24.refs_11_), channel_id=1, source_target_pairs={{0,1},{1,0},{2,3},{3,2},{4,5},{5,4},{6,7},{7,6}} | collective-permute-start | bytes 3145736 | tf_op jit(solution)/shard_map/ppermute | solution.py:683
  436.8 90.7 %collective-permute-start.33 = (bf16[128,4096]{1,0:T(8,128)(2,1)}, bf16[128,4096]{1,0:T(8,128)(2,1)}, u32[]{:S(2)}, u32[]{:S(2)}) collective-permute-start(bf16[128,4096]{1,0:T(8,128)(2,1)} %collective-permute-done.25.refs_12_), channel_id=1, source_target_pairs={{0,1},{1,0},{2,3},{3,2},{4,5},{5,4},{6,7},{7,6}} | collective-permute-start | bytes 3145736 | tf_op jit(solution)/shard_map/ppermute | solution.py:683
  459.2 68.7 %collective-permute-start.34 = (bf16[128,4096]{1,0:T(8,128)(2,1)}, bf16[128,4096]{1,0:T(8,128)(2,1)}, u32[]{:S(2)}, u32[]{:S(2)}) collective-permute-start(bf16[128,4096]{1,0:T(8,128)(2,1)} %collective-permute-done.26.refs_13_), channel_id=1, source_target_pairs={{0,1},{1,0},{2,3},{3,2},{4,5},{5,4},{6,7},{7,6}} | collective-permute-start | bytes 3145736 | tf_op jit(solution)/shard_map/ppermute | solution.py:683
  481.1 44.9 %collective-permute-start.21 = (bf16[256,1024]{1,0:T(8,128)(2,1)}, bf16[256,1024]{1,0:T(8,128)(2,1)}, u32[]{:S(2)}, u32[]{:S(2)}) collective-permute-start(bf16[256,1024]{1,0:T(8,128)(2,1)} %get-tuple-element.97), channel_id=1, source_target_pairs={{0,3},{1,2},{2,1},{3,0},{4,7},{5,6},{6,5},{7,4}} | collective-permute-start | bytes 1572872 | tf_op jit(solution)/shard_map/ppermute | solution.py:683
  563.7 48.8 %collective-permute-start.40 = (bf16[256,4096]{1,0:T(8,128)(2,1)}, bf16[256,4096]{1,0:T(8,128)(2,1)}, u32[]{:S(2)}, u32[]{:S(2)}) collective-permute-start(bf16[256,4096]{1,0:T(8,128)(2,1)} %get-tuple-element.108.refs_0_), channel_id=1, source_target_pairs={{0,1},{1,0},{2,3},{3,2},{4,5},{5,4},{6,7},{7,6}} | collective-permute-start | bytes 6291464 | tf_op jit(solution)/shard_map/ppermute | solution.py:683
  564.1 48.0 %collective-permute-start.39 = (bf16[256,4096]{1,0:T(8,128)(2,1)}, bf16[256,4096]{1,0:T(8,128)(2,1)}, u32[]{:S(2)}, u32[]{:S(2)}) collective-permute-start(bf16[256,4096]{1,0:T(8,128)(2,1)} %get-tuple-element.108.refs_0_), channel_id=1, source_target_pairs={{0,2},{1,3},{2,0},{3,1},{4,6},{5,7},{6,4},{7,5}} | collective-permute-start | bytes 6291464 | tf_op jit(solution)/shard_map/ppermute | solution.py:683
  612.1 109.0 %collective-permute-start.51 = (bf16[256,4096]{1,0:T(8,128)(2,1)}, bf16[256,4096]{1,0:T(8,128)(2,1)}, u32[]{:S(2)}, u32[]{:S(2)}) collective-permute-start(bf16[256,4096]{1,0:T(8,128)(2,1)} %get-tuple-element.124.refs_0_), channel_id=1, source_target_pairs={{0,2},{1,3},{2,0},{3,1},{4,6},{5,7},{6,4},{7,5}} | collective-permute-start | bytes 6291464 | tf_op jit(solution)/shard_map/ppermute | solution.py:683
  705.0 76.3 %collective-permute-start.42 = (bf16[512,4096]{1,0:T(8,128)(2,1)}, bf16[512,4096]{1,0:T(8,128)(2,1)}, u32[]{:S(2)}, u32[]{:S(2)}) collective-permute-start(bf16[512,4096]{1,0:T(8,128)(2,1)} %get-tuple-element.114), channel_id=1, source_target_pairs={{0,1},{1,0},{2,3},{3,2},{4,5},{5,4},{6,7},{7,6}} | collective-permute-start | bytes 12582920 | tf_op jit(solution)/shard_map/ppermute | solution.py:683
  721.0 31.6 %collective-permute-start.48 = (bf16[256,1024]{1,0:T(8,128)(2,1)}, bf16[256,1024]{1,0:T(8,128)(2,1)}, u32[]{:S(2)}, u32[]{:S(2)}) collective-permute-start(bf16[256,1024]{1,0:T(8,128)(2,1)} %get-tuple-element.120), channel_id=1, source_target_pairs={{0,3},{1,2},{2,1},{3,0},{4,7},{5,6},{6,5},{7,4}} | collective-permute-start | bytes 1572872 | tf_op jit(solution)/shard_map/ppermute | solution.py:683
  730.2 55.4 %collective-permute-start.52 = (bf16[256,4096]{1,0:T(8,128)(2,1)}, bf16[256,4096]{1,0:T(8,128)(2,1)}, u32[]{:S(2)}, u32[]{:S(2)}) collective-permute-start(bf16[256,4096]{1,0:T(8,128)(2,1)} %get-tuple-element.124.refs_0_), channel_id=1, source_target_pairs={{0,1},{1,0},{2,3},{3,2},{4,5},{5,4},{6,7},{7,6}} | collective-permute-start | bytes 6291464 | tf_op jit(solution)/shard_map/ppermute | solution.py:683
  731.7 53.9 %collective-permute-start.53 = (bf16[256,4096]{1,0:T(8,128)(2,1)}, bf16[256,4096]{1,0:T(8,128)(2,1)}, u32[]{:S(2)}, u32[]{:S(2)}) collective-permute-start(bf16[256,4096]{1,0:T(8,128)(2,1)} %collective-permute-done.51.refs_1_), channel_id=1, source_target_pairs={{0,1},{1,0},{2,3},{3,2},{4,5},{5,4},{6,7},{7,6}} | collective-permute-start | bytes 6291464 | tf_op jit(solution)/shard_map/ppermute | solution.py:683
  874.2 48.5 %collective-permute-start.56 = (bf16[512,4096]{1,0:T(8,128)(2,1)}, bf16[512,4096]{1,0:T(8,128)(2,1)S(1)}, u32[]{:S(2)}, u32[]{:S(2)}) collective-permute-start(bf16[512,4096]{1,0:T(8,128)(2,1)} %get-tuple-element.128), channel_id=1, source_target_pairs={{0,1},{1,0},{2,3},{3,2},{4,5},{5,4},{6,7},{7,6}} | collective-permute-start | bytes 12582920 | tf_op jit(solution)/shard_map/ppermute | solution.py:683
  874.8 47.8 %collective-permute-start.50 = (bf16[256,4096]{1,0:T(8,128)(2,1)}, bf16[256,4096]{1,0:T(8,128)(2,1)S(1)}, u32[]{:S(2)}, u32[]{:S(2)}) collective-permute-start(bf16[256,4096]{1,0:T(8,128)(2,1)} %get-tuple-element.123.refs_0_), channel_id=1, source_target_pairs={{0,2},{1,3},{2,0},{3,1},{4,6},{5,7},{6,4},{7,5}} | collective-permute-start | bytes 6291464 | tf_op jit(solution)/shard_map/ppermute | solution.py:683
  875.3 52.7 %collective-permute-start.54 = (bf16[256,4096]{1,0:T(8,128)(2,1)}, bf16[256,4096]{1,0:T(8,128)(2,1)S(1)}, u32[]{:S(2)}, u32[]{:S(2)}) collective-permute-start(bf16[256,4096]{1,0:T(8,128)(2,1)} %get-tuple-element.123.refs_0_), channel_id=1, source_target_pairs={{0,1},{1,0},{2,3},{3,2},{4,5},{5,4},{6,7},{7,6}} | collective-permute-start | bytes 6291464 | tf_op jit(solution)/shard_map/ppermute | solution.py:683
  1017.8 71.7 %collective-permute-start.61 = (bf16[512,4096]{1,0:T(8,128)(2,1)}, bf16[512,4096]{1,0:T(8,128)(2,1)}, u32[]{:S(2)}, u32[]{:S(2)}) collective-permute-start(bf16[512,4096]{1,0:T(8,128)(2,1)} %get-tuple-element.134), channel_id=1, source_target_pairs={{0,1},{1,0},{2,3},{3,2},{4,5},{5,4},{6,7},{7,6}} | collective-permute-start | bytes 12582920 | tf_op jit(solution)/shard_map/ppermute | solution.py:683
  1018.2 48.8 %collective-permute-start.49 = (bf16[256,4096]{1,0:T(8,128)(2,1)}, bf16[256,4096]{1,0:T(8,128)(2,1)}, u32[]{:S(2)}, u32[]{:S(2)}) collective-permute-start(bf16[256,4096]{1,0:T(8,128)(2,1)} %add_convert_fusion.2.refs_7_), channel_id=1, source_target_pairs={{0,2},{1,3},{2,0},{3,1},{4,6},{5,7},{6,4},{7,5}} | collective-permute-start | bytes 6291464 | tf_op jit(solution)/shard_map/ppermute | solution.py:683
  1018.6 70.9 %collective-permute-start.58 = (bf16[128,4096]{1,0:T(8,128)(2,1)}, bf16[128,4096]{1,0:T(8,128)(2,1)}, u32[]{:S(2)}, u32[]{:S(2)}) collective-permute-start(bf16[128,4096]{1,0:T(8,128)(2,1)} %get-tuple-element.131.refs_0_), channel_id=1, source_target_pairs={{0,2},{1,3},{2,0},{3,1},{4,6},{5,7},{6,4},{7,5}} | collective-permute-start | bytes 3145736 | tf_op jit(solution)/shard_map/ppermute | solution.py:683
  1020.2 73.6 %collective-permute-start.59 = (bf16[128,4096]{1,0:T(8,128)(2,1)}, bf16[128,4096]{1,0:T(8,128)(2,1)}, u32[]{:S(2)}, u32[]{:S(2)}) collective-permute-start(bf16[128,4096]{1,0:T(8,128)(2,1)} %get-tuple-element.131.refs_0_), channel_id=1, source_target_pairs={{0,1},{1,0},{2,3},{3,2},{4,5},{5,4},{6,7},{7,6}} | collective-permute-start | bytes 3145736 | tf_op jit(solution)/shard_map/ppermute | solution.py:683
  1020.2 148.2 %collective-permute-start.57 = (bf16[256,4096]{1,0:T(8,128)(2,1)}, bf16[256,4096]{1,0:T(8,128)(2,1)}, u32[]{:S(2)}, u32[]{:S(2)}) collective-permute-start(bf16[256,4096]{1,0:T(8,128)(2,1)} %add_convert_fusion.1.refs_7_), channel_id=1, source_target_pairs={{0,2},{1,3},{2,0},{3,1},{4,6},{5,7},{6,4},{7,5}} | collective-permute-start | bytes 6291464 | tf_op jit(solution)/shard_map/ppermute | solution.py:683
  1142.1 32.0 %collective-permute-start.66 = (bf16[256,4096]{1,0:T(8,128)(2,1)}, bf16[256,4096]{1,0:T(8,128)(2,1)}, u32[]{:S(2)}, u32[]{:S(2)}) collective-permute-start(bf16[256,4096]{1,0:T(8,128)(2,1)} %get-tuple-element.139), channel_id=1, source_target_pairs={{0,1},{1,0},{2,3},{3,2},{4,5},{5,4},{6,7},{7,6}} | collective-permute-start | bytes 6291464 | tf_op jit(solution)/shard_map/ppermute | solution.py:683
  1142.6 25.4 %collective-permute-start.63 = (bf16[128,4096]{1,0:T(8,128)(2,1)}, bf16[128,4096]{1,0:T(8,128)(2,1)}, u32[]{:S(2)}, u32[]{:S(2)}) collective-permute-start(bf16[128,4096]{1,0:T(8,128)(2,1)} %get-tuple-element.136.refs_0_), channel_id=1, source_target_pairs={{0,2},{1,3},{2,0},{3,1},{4,6},{5,7},{6,4},{7,5}} | collective-permute-start | bytes 3145736 | tf_op jit(solution)/shard_map/ppermute | solution.py:683
  1143.0 33.8 %collective-permute-start.64 = (bf16[128,4096]{1,0:T(8,128)(2,1)}, bf16[128,4096]{1,0:T(8,128)(2,1)}, u32[]{:S(2)}, u32[]{:S(2)}) collective-permute-start(bf16[128,4096]{1,0:T(8,128)(2,1)} %get-tuple-element.136.refs_0_), channel_id=1, source_target_pairs={{0,1},{1,0},{2,3},{3,2},{4,5},{5,4},{6,7},{7,6}} | collective-permute-start | bytes 3145736 | tf_op jit(solution)/shard_map/ppermute | solution.py:683
  1168.0 58.6 %collective-permute-start.62 = (bf16[256,4096]{1,0:T(8,128)(2,1)}, bf16[256,4096]{1,0:T(8,128)(2,1)}, u32[]{:S(2)}, u32[]{:S(2)}) collective-permute-start(bf16[256,4096]{1,0:T(8,128)(2,1)} %add_convert_fusion.refs_7_), channel_id=1, source_target_pairs={{0,2},{1,3},{2,0},{3,1},{4,6},{5,7},{6,4},{7,5}} | collective-permute-start | bytes 6291464 | tf_op jit(solution)/shard_map/ppermute | solution.py:683
  1225.0 26.3 %collective-permute-start.67 = (bf16[128,4096]{1,0:T(8,128)(2,1)}, bf16[128,4096]{1,0:T(8,128)(2,1)}, u32[]{:S(2)}, u32[]{:S(2)}) collective-permute-start(bf16[128,4096]{1,0:T(8,128)(2,1)} %add_convert_fusion.4.refs_7_), channel_id=1, source_target_pairs={{0,2},{1,3},{2,0},{3,1},{4,6},{5,7},{6,4},{7,5}} | collective-permute-start | bytes 3145736 | tf_op jit(solution)/shard_map/ppermute | solution.py:683
  1235.0 38.1 %collective-permute-start.69 = (bf16[128,4096]{1,0:T(8,128)(2,1)}, bf16[128,4096]{1,0:T(8,128)(2,1)}, u32[]{:S(2)}, u32[]{:S(2)}) collective-permute-start(bf16[128,4096]{1,0:T(8,128)(2,1)} %add_convert_fusion.3.refs_5_), channel_id=1, source_target_pairs={{0,2},{1,3},{2,0},{3,1},{4,6},{5,7},{6,4},{7,5}} | collective-permute-start | bytes 3145736 | tf_op jit(solution)/shard_map/ppermute | solution.py:683
  (27 other events, 263.8 us)

commit v7 on v6

--- a/solution.py
+++ b/solution.py
@@ -377,8 +377,8 @@
     )(tab, *qs, *kvs, *sts, *after)
 
 
-def out_kernel(*refs, blocks, n_w, n_run, at, parts):
-    n_o, n_out = 4 * n_run, 2 * len(parts)
+def out_kernel(*refs, blocks, n_w, n_run, at):
+    n_o, n_out = 4 * n_run, 2 * n_run
     o_refs, w_refs, x_ref, g_ref = refs[:n_o], refs[n_o:n_o + n_w], refs[n_o + n_w], refs[n_o + n_w + 1]
     outs = refs[n_o + n_w + 2:n_o + n_w + 2 + n_out]
     o_scr, w_scr, x_scr, acc_scr, o_sem, w_sem, x_sem, out_sem = refs[n_o + n_w + 2 + n_out:]
@@ -443,55 +443,57 @@
         o_scr[rows, :] = norm_rows(y, g_ref[...])
         return carry
 
-    stores, r0 = [], 0
-    for i, n in enumerate(parts):
-        lax.fori_loop(r0 // 32, (r0 + n) // 32, rows32, 0)
+    stores, per = [], RUN // 32
+    for i in range(n_run):
+        lax.fori_loop(i * per, (i + 1) * per, rows32, 0)
         for k, scr in enumerate((x_scr, o_scr)):
-            stores.append(pltpu.make_async_copy(scr.at[pl.ds(r0, n), :], outs[2 * i + k], out_sem.at[2 * i + k]))
+            stores.append(pltpu.make_async_copy(scr.at[pl.ds(i * RUN, RUN), :], outs[2 * i + k], out_sem.at[2 * i + k]))
             stores[-1].start()
-        r0 += n
     for cp in stores:
         cp.wait()
 
 
-def out_proj(os, ws, blocks, x_rows, gain, at, parts, after=()):
+def out_proj(os, ws, blocks, x_rows, gain, at, after=()):
     dim = x_rows.shape[1]
     width = os[0].shape[1]
     n_run = len(os) // 4
     rows = n_run * RUN
     return pl.pallas_call(
-        ordered(functools.partial(out_kernel, blocks=blocks, n_w=len(ws), n_run=n_run, at=at, parts=parts),
+        ordered(functools.partial(out_kernel, blocks=blocks, n_w=len(ws), n_run=n_run, at=at),
                 len(os) + len(ws) + 2, after),
         grid=(1,),
         in_specs=[ANY] * (len(os) + len(ws) + 1) + [pl.BlockSpec((1, dim), lambda i: (0, 0))] + [ANY] * len(after),
-        out_specs=[ANY] * (2 * len(parts)),
-        out_shape=[jax.ShapeDtypeStruct((n, dim), BF) for n in parts for _ in range(2)],
+        out_specs=[ANY] * (2 * n_run),
+        out_shape=[jax.ShapeDtypeStruct((RUN, dim), BF)] * (2 * n_run),
         scratch_shapes=[pltpu.VMEM((rows, 4 * width), BF), pltpu.VMEM((3, width // 2, dim), BF), pltpu.VMEM((rows, dim), BF),
                         pltpu.VMEM((rows, dim), F32), pltpu.SemaphoreType.DMA((len(blocks), 2 * n_run)),
-                        pltpu.SemaphoreType.DMA((3,)), pltpu.SemaphoreType.DMA, pltpu.SemaphoreType.DMA((2 * len(parts),))],
+                        pltpu.SemaphoreType.DMA((3,)), pltpu.SemaphoreType.DMA, pltpu.SemaphoreType.DMA((2 * n_run,))],
         name="outp", compiler_params=params(1),
         cost_estimate=cost(8 * rows * width * dim, 8 * width * dim),
     )(*os, *ws, x_rows, gain, *after)
 
 
-def mlp_kernel(*refs, n_in, tn, td, nk, nd):
+def mlp_kernel(*refs, n_in, first, rb, tn, td, nk, nd):
     b_refs = refs[:n_in]
     wg_ref, wu_ref, wd_ref, keep_ref, send_ref, b_scr, u_scr, w_scr, d_scr, b_sem, w_sem, d_sem = refs[n_in:]
     i = pl.program_id(0)
-    rb = b_refs[0].shape[0]
 
     def fetch(j):
+        def tile(src, dst, sem):
+            part = src.shape[0] // 4
+            for r in range(0, src.shape[0], part):
+                pltpu.make_async_copy(src.at[pl.ds(r, part), :], dst.at[pl.ds(r, part), :], sem).start()
+
         @pl.when(j < nk)
         def _():
             cols = pl.ds(pl.multiple_of(j * tn, tn), tn)
             for k, w in enumerate((wg_ref, wu_ref)):
-                pltpu.make_async_copy(w.at[:, cols], w_scr.at[lax.rem(j, 2), k], w_sem.at[lax.rem(j, 2)]).start()
+                tile(w.at[:, cols], w_scr.at[lax.rem(j, 2), k], w_sem.at[lax.rem(j, 2)])
 
         @pl.when((j >= nk) & (j < nk + nd))
         def _():
             n = j - nk
-            pltpu.make_async_copy(wd_ref.at[:, pl.ds(pl.multiple_of(n * td, td), td)], d_scr.at[lax.rem(n, 2)],
-                                  d_sem.at[lax.rem(n, 2)]).start()
+            tile(wd_ref.at[:, pl.ds(pl.multiple_of(n * td, td), td)], d_scr.at[lax.rem(n, 2)], d_sem.at[lax.rem(n, 2)])
 
     def gated(rows, cols, slot):
         b = b_scr[rows, :]
@@ -501,7 +503,8 @@
 
     @pl.when(i == 0)
     def _():
-        copies = [pltpu.make_async_copy(r, b_scr.at[pl.ds(k * rb, rb), :], b_sem.at[k]) for k, r in enumerate(b_refs)]
+        copies = [pltpu.make_async_copy(r.at[pl.ds(first, rb), :], b_scr.at[pl.ds(k * rb, rb), :], b_sem.at[k])
+                  for k, r in enumerate(b_refs)]
         copies[0].start()
         fetch(i)
         for cp in copies[1:]:
@@ -537,15 +540,16 @@
         send_ref[...] = d[half:]
 
 
-def mlp(bs, wg, wu, wd, after=()):
-    rb, dim = bs[0].shape
+def mlp(bs, first, rb, wg, wu, wd, after=()):
+    dim = bs[0].shape[1]
     rows = rb * len(bs)
     ffn = wg.shape[1]
-    tn, td = (256, 256) if rows > 512 else (512, 512)
+    td = 512
+    tn = td if rows <= td else td // 2
     nk, nd = ffn // tn, dim // td
     dn = lambda i: (0, jnp.maximum(i - nk, 0))
     return pl.pallas_call(
-        ordered(functools.partial(mlp_kernel, n_in=len(bs), tn=tn, td=td, nk=nk, nd=nd), len(bs) + 3, after),
+        ordered(functools.partial(mlp_kernel, n_in=len(bs), first=first, rb=rb, tn=tn, td=td, nk=nk, nd=nd), len(bs) + 3, after),
         grid=(nk + nd,),
         in_specs=[ANY] * (len(bs) + 3 + len(after)),
         out_specs=[pl.BlockSpec((rows // 2, td), dn)] * 2,
@@ -564,14 +568,14 @@
     z_ref[...] = (y_ref[...].astype(F32) + total.astype(BF).astype(F32)).astype(BF)
 
 
-def sum_rows(z, keep, recv, far, y, first, total, after=(), tile=64):
-    rows, dim = y.shape
-    spec = pl.BlockSpec((tile, dim), lambda i: (i, 0))
+def sum_rows(z, keep, recv, far, y, y_first, rows, first, total, after=(), tile=64):
+    dim = y.shape[1]
+    at = lambda r0: pl.BlockSpec((tile, dim), lambda i: (r0 // tile + i, 0))
     prev = () if z is None else (z,)
     return pl.pallas_call(
         ordered(sum_kernel, len(prev) + 4, after), grid=(rows // tile,),
-        in_specs=[ANY] * len(prev) + [spec] * 4 + [ANY] * len(after),
-        out_specs=pl.BlockSpec((tile, dim), lambda i: (first // tile + i, 0)),
+        in_specs=[ANY] * len(prev) + [at(0)] * 3 + [at(y_first)] + [ANY] * len(after),
+        out_specs=at(first),
         out_shape=jax.ShapeDtypeStruct((total, dim), BF),
         input_output_aliases={0: 0} if prev else {},
         name="zsum", compiler_params=params(1),
@@ -644,7 +648,13 @@
                     pairs, carry = [], []
                     for t in tiles:
                         seen = [r for r in range(len(pos)) if pos[r] < pos[t]]
-                        pairs.append(([r for r in seen if max(stage(r), stage(t)) == now], stage(t) == now))
+                        when = {r: max(stage(r), stage(t)) for r in seen}
+                        late = list(when.values()).count(1) + stage(t)
+                        soon = len(seen) + 1 - late
+                        if late and soon % 4 <= -late % 4:
+                            for r in [r for r in seen if not when[r]][:soon % 4]:
+                                when[r] = 1
+                        pairs.append(([r for r in seen if when[r] == now], stage(t) == now))
                         carry.append(int(stage(t) < now))
                     tab, n = call_table(tiles, pos, pairs, carry, 2 if now == 1 else 0)
                     tabs[-1].append(tab)
@@ -673,8 +683,7 @@
         np_tab, np_runs, bases, work = work_tables(cps, piece)
         dev = y_id * n_tp + t_id
         tab = lax.dynamic_index_in_dim(jnp.asarray(np_tab), dev, 0, keepdims=False)
-        order = list(range(2 * n_run)) + [2 * n_run + i for i in (2, 3, 4, 5, 0, 1, 6, 7)]
-        run_pos = lax.dynamic_index_in_dim(jnp.asarray(np_runs[:, order]), dev, 0, keepdims=False)
+        run_pos = lax.dynamic_index_in_dim(jnp.asarray(np_runs), dev, 0, keepdims=False)
 
         def tied(v, *others):
             return lax.optimization_barrier((v, *others))[0]
@@ -692,34 +701,34 @@
         w_all = jnp.concatenate([tied(w, own[-1]).reshape(dim, -1) for w in (w_q, w_k, w_v)], axis=1)
         tables = rope_tables(tied(run_pos, own[-1])[:, None] + jnp.arange(RUN, dtype=jnp.int32)[None, :])
 
-        def relayed(j, after):
+        q_here, kv_here = qkv(own + mate, w_all, (tables, 0))
+        kvs, q_far = [kv_here], []
+
+        def far_qkv(j, after):
             here = tied(far[j], after)
-            return [here, send(over_core, here)]
-
-        q_here, kv_here = qkv(own + mate, w_all, (tables, 0))
-        q_a, kv_a = qkv(relayed(0, kv_here), w_all, (tables, 2 * n_run + 4), after=(kv_here,))
+            q, kv = qkv([here, send(over_core, here)], w_all, (tables, 2 * (n_run + j)), after=(after,))
+            q_far.append(q)
+            kvs.append(kv)
+            return kv
+
+        far_qkv(1, far_qkv(0, kv_here))
 
         wo = w_o.reshape(-1, dim)
         half = wo.shape[0] // 2
-        n_piece = n_run
+        n_piece = 2
         rows = half // n_piece
-        wo_gated = tied(wo, kv_a)
+        wo_gated = tied(wo, kvs[-1])
         wo_x = [send(over_x, lax.dynamic_slice_in_dim(wo_gated, y_id * half + p * rows, rows, axis=0))
                 for p in range(n_piece)]
         wo_c = send(over_core, wo_gated)
-        early = relayed(1, kv_a)
-
-        tile = lambda a, n: [(a, i) for i in range(n)]
-        tiles = tile(0, 2 * n_run) + tile(1, 2)
-        st, = flash(tab, [q_here, q_a], tiles, [kv_here, kv_a], base=bases[0], work=int(work[0]),
-                   st_tiles=len(tiles))
-        q_b, kv_b = qkv(early + relayed(2, st), w_all, (tables, 2 * n_run), after=(st,))
-        q_c, kv_c = qkv(relayed(3, kv_b), w_all, (tables, 2 * n_run + 6), after=(kv_b,))
-        kvs = [kv_here, kv_a, kv_b, kv_c]
+
+        tiles = [(0, i) for i in range(2 * n_run)] + [(1, 0), (1, 1)]
+        st, = flash(tab, [q_here, q_far[0]], tiles, kvs[:2], base=bases[0], work=int(work[0]),
+                   st_tiles=len(tiles), after=(kvs[-1],))
+        far_qkv(3, far_qkv(2, st))
         kvs = kvs + [send(over_y, kv) for kv in kvs]
-        q_far = [(q_a, 0), (q_b, 0), (q_b, 2), (q_c, 0)]
-
-        os, outs, prev = [], [], kv_c
+
+        os, outs, prev = [], [], kvs[n_run]
         wo_a, wo_ya, wo_yb = {}, {}, {}
 
         def forward_w(p):
@@ -732,11 +741,10 @@
             wo_yb[p] = (here, send(over_core, here))
 
         def attend(j):
-            q, at = q_far[j]
             held = 2 * n_run + 2 * j
             carried = [j, n_run + j] + ([held, held + 1] if j == 0 else [None, None])
             o_own, o_mate, o_far, o_fm = flash(
-                tab, [q_here, q], [(0, j), (0, n_run + j), (1, at), (1, at + 1)], kvs,
+                tab, [q_here, q_far[j]], [(0, j), (0, n_run + j), (1, 0), (1, 1)], kvs,
                 base=bases[1 + j], work=int(work[1 + j]), st=st, st_src=carried, after=(prev,))
             os.append([o_own, send(over_core, o_mate), send(over_x, o_far), send(over_both, o_fm)])
             return o_own
@@ -748,22 +756,18 @@
                 for held in (wo_ya, wo_yb):
                     blocks.append([(len(ws) + p, 0, rows) for p in range(n_piece)])
                     ws += [held[p][k] for p in range(n_piece)]
-            parts = (RUN, RUN) if i == 0 else (RUN, RUN // 2, RUN // 2)
-            got = out_proj(os[2 * i] + os[2 * i + 1], ws, blocks, x_rows, gm, i, parts, after=(prev,))
+            got = out_proj(os[2 * i] + os[2 * i + 1], ws, blocks, x_rows, gm, i, after=(prev,))
             for y, b in zip(got[::2], got[1::2]):
                 outs.append((y, b, send(over_x, b), send(over_core, b)))
             return got[0]
 
         last = n_run - 1
         for j in range(last):
-            forward_w(j)
+            prev = attend(j)
+            if j < n_piece:
+                forward_w(j)
             if j:
                 relay_w(j - 1)
-            if j == last - 1:
-                forward_w(last)
-            prev = attend(j)
-        for p in range(last - 1, n_piece):
-            relay_w(p)
         prev = project(0)
         prev = attend(last)
 
@@ -773,31 +777,30 @@
             here = tied(outs[j][2], prev)
             relay[j] = (here, send(over_core, here))
 
-        def finish(j):
-            first = sum(o[0].shape[0] for o in outs[:j])
-            return sum_rows(z, *sums[j], first, n_run * RUN, after=() if prev is z else (prev,))
+        chunks = [(j, 0, RUN) for j in range(last)] + [(last, 0, RUN // 2), (last, RUN // 2, RUN // 2)]
+
+        def finish(c):
+            j, first, size = chunks[c]
+            return sum_rows(z, *sums[c], outs[j][0], first, size, j * RUN + first, n_run * RUN,
+                        after=() if prev is z else (prev,))
 
         relay_b(0)
-        n_part = n_run + 1
-        for j in range(n_part):
-            y, b, _, b_mate = outs[j]
-            keep, out = mlp([b, relay[j][0], b_mate, relay[j][1]], w_gate, w_up, w_down, after=(prev,))
+        for c, (j, first, size) in enumerate(chunks):
+            b = [outs[j][1], relay[j][0], outs[j][3], relay[j][1]]
+            keep, out = mlp(b, first, size, w_gate, w_up, w_down, after=(prev,))
             recv = send(over_core, out)
             prev = keep
-            if j == 0:
-                relay_b(1)
+            if c < last:
+                relay_b(c + 1)
+            if c == 0:
                 prev = project(1)
-            else:
-                if j + 1 < n_part:
-                    relay_b(j + 1)
-                if j > 1:
-                    prev = z = finish(j - 2)
+            elif c > 1:
+                prev = z = finish(c - 2)
             kept = keep if prev is keep else tied(keep, prev)
-            half = y.shape[0]
-            prev = s_far = (kept[half:].astype(F32) + recv[half:].astype(F32)).astype(BF)
-            sums.append((keep, recv, send(over_x, s_far), y))
-        for j in (n_part - 2, n_part - 1):
-            prev = z = finish(j)
+            prev = s_far = (kept[size:].astype(F32) + recv[size:].astype(F32)).astype(BF)
+            sums.append((keep, recv, send(over_x, s_far)))
+        for c in (last, n_run):
+            prev = z = finish(c)
         return z[None]
 
     return jax.shard_map(layer, mesh=mesh,

time: 1290 us -> 1330 us (1.031)
  waiting for transfers between devices: 417 us -> 441 us
  starting transfers between devices: 48.6 us -> 63.4 us
    ppermute x70 -> x60, waiting for transfers between devices: 417 us -> 441 us  [send(): return lax.ppermute(v, *axis_pairs)]
    ppermute x70 -> x60, starting transfers between devices: 48.6 us -> 63.4 us  [send(): return lax.ppermute(v, *axis_pairs)]
    pallas_call x4 -> x5, Pallas kernels: 90.6 us -> 96.4 us  [qkv(): pl.pallas_call(ordered(functools.partial(qkv_kernel, n_in=n_in, n_q=n_q,...]
  transfers between devices with their start and end apart: 70 -> 60, of which waited for: 30 -> 30; matrix products, arithmetic and copies ran while one was open for 4% -> 3% of each run, Pallas kernels for 43% -> 42%
where the time goes in v7:
time: 1330 us; the launch traced here: 1320 us
  Pallas kernels  770 us (58%)
  waiting for transfers between devices  441 us (33%)
  starting transfers between devices  63.4 us (5%)
  other arithmetic  24.5 us (2%)
  local copies, waits for them, and re-layouts  23.9 us (2%)
    ppermute x60, waiting for transfers between devices, send(): return lax.ppermute(v, *axis_pairs)  441 us
    pallas_call x5, Pallas kernels, mlp(): pl.pallas_call(ordered(functools.partial(mlp_kernel, n_in=len(bs), first=...  364 us
    pallas_call x5, Pallas kernels, flash(): pl.pallas_call(ordered(functools.partial(flash_kernel, q_src=q_src, kv_sr...  215 us
    pallas_call x5, Pallas kernels, qkv(): pl.pallas_call(ordered(functools.partial(qkv_kernel, n_in=n_in, n_q=n_q,...  96.4 us
    ppermute x60, starting transfers between devices, send(): return lax.ppermute(v, *axis_pairs)  63.4 us
    pallas_call x2, Pallas kernels, out_proj(): pl.pallas_call(ordered(functools.partial(out_kernel, blocks=blocks, n_w=l...  58 us
  transfers between devices with their start and end apart: 60, of which 30 were waited for; matrix products, arithmetic and copies ran while one was open for 3% of the time, Pallas kernels for 42%

profile of v7, /device:TPU:0, one launch (start us, length us, event | category | flops | bytes accessed | tf_op | source)
XLA Modules:
  0.0 1324.0 jit_solution(10238729097359361753)
XLA Ops:
  20.0 9.3 bitcast_dynamic-update-slice_fusion
  29.3 4.8 multiply_sine_fusion
  38.0 39.7 %qkv.5 = (bf16[8,1024,256]{2,1,0:T(8,128)(2,1)}, bf16[8,2,256,256]{3,2,1,0:T(8,128)(2,1)}) custom-call(bf16[256,4096]{1,0:T(8,128)(2,1)} %norm.4.refs_2_.refs_0_, bf16[256,4096]{1,0:T(8,128)(2,1)} %norm.5.refs_2_.refs_1_, bf16[256,4096]{1,0:T(8,128)(2,1)} %norm.6.refs_2_, bf16[256,4096]{1,0:T(8,128)(2,1)} %norm.7.refs_3_, ...), custom_call_target="tpu_custom_call" | custom-call | flops 25769803776 | bytes 12582912 | tf_op jit(solution)/shard_map/qkv/pallas_call | solution.py:124
  77.8 4.5 collective-permute-done.5.refs_1_
  82.3 14.1 %qkv.6 = (bf16[2,1024,256]{2,1,0:T(8,128)(2,1)}, bf16[2,2,256,256]{3,2,1,0:T(8,128)(2,1)}) custom-call(bf16[256,4096]{1,0:T(8,128)(2,1)} %collective-permute-done.4.refs_0_, bf16[256,4096]{1,0:T(8,128)(2,1)} %collective-permute-done.5.refs_1_, bf16[4096,1536]{1,0:T(8,128)(2,1)} %bitcast_dynamic-update-slice_fusion.1.refs_8_.refs_2_, ...), custom_call_target="tpu_custom_call" | custom-call | flops 6442450944 | bytes 12582912 | tf_op jit(solution)/shard_map/qkv/pallas_call | solution.py:124
  96.4 29.7 %collective-permute-done.6.refs_0_ = bf16[256,4096]{1,0:T(8,128)(2,1)} collective-permute-done((bf16[256,4096]{1,0:T(8,128)(2,1)}, bf16[256,4096]{1,0:T(8,128)(2,1)}, u32[]{:S(2)}, u32[]{:S(2)}) %collective-permute-start.6) | collective-permute-done | bytes 2097184 | tf_op jit(solution)/shard_map/ppermute | solution.py:692
  130.7 14.4 %qkv.7 = (bf16[2,1024,256]{2,1,0:T(8,128)(2,1)}, bf16[2,2,256,256]{3,2,1,0:T(8,128)(2,1)}) custom-call(bf16[256,4096]{1,0:T(8,128)(2,1)} %collective-permute-done.6.refs_0_, bf16[256,4096]{1,0:T(8,128)(2,1)} %collective-permute-done.7.refs_1_, bf16[4096,1536]{1,0:T(8,128)(2,1)} %bitcast_dynamic-update-slice_fusion.1.refs_8_.refs_2_, ...), custom_call_target="tpu_custom_call" | custom-call | flops 6442450944 | bytes 12582912 | tf_op jit(solution)/shard_map/qkv/pallas_call | solution.py:124
  145.0 52.9 %flash_part.1.refs_5_.refs_13_ = f32[10,2,4,144,256]{4,3,2,1,0:T(8,128)} custom-call(s32[969]{0:T(1024)} %bitcast.28, bf16[8,1024,256]{2,1,0:T(8,128)(2,1)} %get-tuple-element.74.refs_1_, bf16[2,1024,256]{2,1,0:T(8,128)(2,1)} %get-tuple-element.77.refs_2_, bf16[8,2,256,256]{3,2,1,0:T(8,128)(2,1)} %get-tuple-element.75.refs_5_.refs_3_, ...), custom_call_target="tpu_custom_call" | custom-call | flops 38654705664 | bytes 2621440 | tf_op jit(solution)/shard_map/flash_part/pallas_call | solution.py:351
  203.8 14.2 %qkv.8 = (bf16[2,1024,256]{2,1,0:T(8,128)(2,1)}, bf16[2,2,256,256]{3,2,1,0:T(8,128)(2,1)}) custom-call(bf16[256,4096]{1,0:T(8,128)(2,1)} %collective-permute-done.8.refs_0_, bf16[256,4096]{1,0:T(8,128)(2,1)} %collective-permute-done.9.refs_1_, bf16[4096,1536]{1,0:T(8,128)(2,1)} %bitcast_dynamic-update-slice_fusion.1.refs_8_.refs_2_, ...), custom_call_target="tpu_custom_call" | custom-call | flops 6442450944 | bytes 12582912 | tf_op jit(solution)/shard_map/qkv/pallas_call | solution.py:124
  218.0 29.6 %collective-permute-done.10.refs_0_ = bf16[256,4096]{1,0:T(8,128)(2,1)} collective-permute-done((bf16[256,4096]{1,0:T(8,128)(2,1)}, bf16[256,4096]{1,0:T(8,128)(2,1)}, u32[]{:S(2)}, u32[]{:S(2)}) %collective-permute-start.10) | collective-permute-done | bytes 2097184 | tf_op jit(solution)/shard_map/ppermute | solution.py:692
  252.1 14.1 %qkv.9 = (bf16[2,1024,256]{2,1,0:T(8,128)(2,1)}, bf16[2,2,256,256]{3,2,1,0:T(8,128)(2,1)}) custom-call(bf16[256,4096]{1,0:T(8,128)(2,1)} %collective-permute-done.10.refs_0_, bf16[256,4096]{1,0:T(8,128)(2,1)} %collective-permute-done.11.refs_1_, bf16[4096,1536]{1,0:T(8,128)(2,1)} %bitcast_dynamic-update-slice_fusion.1.refs_8_.refs_2_, ...), custom_call_target="tpu_custom_call" | custom-call | flops 6442450944 | bytes 12582912 | tf_op jit(solution)/shard_map/qkv/pallas_call | solution.py:124
  267.7 4.8 constant_dynamic-slice_fusion
  272.5 23.9 %collective-permute-done.12.refs_8_ = bf16[8,2,256,256]{3,2,1,0:T(8,128)(2,1)} collective-permute-done((bf16[8,2,256,256]{3,2,1,0:T(8,128)(2,1)}, bf16[8,2,256,256]{3,2,1,0:T(8,128)(2,1)}, u32[]{:S(2)}, u32[]{:S(2)}) %collective-permute-start.12) | collective-permute-done | bytes 2097184 | tf_op jit(solution)/shard_map/ppermute | solution.py:692
  296.4 11.2 collective-permute-done.13.refs_9_
  307.9 10.9 collective-permute-done.14.refs_10_
  319.2 10.9 collective-permute-done.15.refs_11_
  330.1 10.8 collective-permute-done.16.refs_12_
  340.9 29.3 %flash.4 = (bf16[256,1024]{1,0:T(8,128)(2,1)}, bf16[256,1024]{1,0:T(8,128)(2,1)}, bf16[256,1024]{1,0:T(8,128)(2,1)}, bf16[256,1024]{1,0:T(8,128)(2,1)}) custom-call(s32[969]{0:T(1024)} %bitcast.29, bf16[8,1024,256]{2,1,0:T(8,128)(2,1)} %get-tuple-element.74.refs_1_, bf16[2,1024,256]{2,1,0:T(8,128)(2,1)} %get-tuple-element.77.refs_2_, ...), custom_call_target="tpu_custom_call" | custom-call | flops 27917287424 | bytes 8388608 | tf_op jit(solution)/shard_map/flash/pallas_call | solution.py:351
  370.2 44.6 %flash.5 = (bf16[256,1024]{1,0:T(8,128)(2,1)}, bf16[256,1024]{1,0:T(8,128)(2,1)}, bf16[256,1024]{1,0:T(8,128)(2,1)}, bf16[256,1024]{1,0:T(8,128)(2,1)}) custom-call(s32[969]{0:T(1024)} %bitcast.30, bf16[8,1024,256]{2,1,0:T(8,128)(2,1)} %get-tuple-element.74.refs_1_, bf16[2,1024,256]{2,1,0:T(8,128)(2,1)} %get-tuple-element.89.refs_2_, ...), custom_call_target="tpu_custom_call" | custom-call | flops 32212254720 | bytes 8388608 | tf_op jit(solution)/shard_map/flash/pallas_call | solution.py:351
  416.8 11.5 collective-permute-start.18
  430.3 11.1 collective-permute-done.18.refs_2_
  441.4 22.2 %collective-permute-done.27.refs_13_ = bf16[256,4096]{1,0:T(8,128)(2,1)} collective-permute-done((bf16[256,4096]{1,0:T(8,128)(2,1)}, bf16[256,4096]{1,0:T(8,128)(2,1)}, u32[]{:S(2)}, u32[]{:S(2)}) %collective-permute-start.27) | collective-permute-done | bytes 2097184 | tf_op jit(solution)/shard_map/ppermute | solution.py:692
  463.6 11.5 collective-permute-start.21
  475.1 32.1 %collective-permute-done.26.refs_12_ = bf16[256,4096]{1,0:T(8,128)(2,1)} collective-permute-done((bf16[256,4096]{1,0:T(8,128)(2,1)}, bf16[256,4096]{1,0:T(8,128)(2,1)}, u32[]{:S(2)}, u32[]{:S(2)}) %collective-permute-start.26) | collective-permute-done | bytes 2097184 | tf_op jit(solution)/shard_map/ppermute | solution.py:692
  507.2 11.2 collective-permute-start.22
  518.4 44.2 %flash.6 = (bf16[256,1024]{1,0:T(8,128)(2,1)}, bf16[256,1024]{1,0:T(8,128)(2,1)}, bf16[256,1024]{1,0:T(8,128)(2,1)}, bf16[256,1024]{1,0:T(8,128)(2,1)}) custom-call(s32[969]{0:T(1024)} %bitcast.31, bf16[8,1024,256]{2,1,0:T(8,128)(2,1)} %get-tuple-element.74.refs_1_, bf16[2,1024,256]{2,1,0:T(8,128)(2,1)} %get-tuple-element.98.refs_2_, ...), custom_call_target="tpu_custom_call" | custom-call | flops 32212254720 | bytes 8388608 | tf_op jit(solution)/shard_map/flash/pallas_call | solution.py:351
  576.8 29.0 %outp.2 = (bf16[256,4096]{1,0:T(8,128)(2,1)}, bf16[256,4096]{1,0:T(8,128)(2,1)}, bf16[256,4096]{1,0:T(8,128)(2,1)}, bf16[256,4096]{1,0:T(8,128)(2,1)}) custom-call(bf16[256,1024]{1,0:T(8,128)(2,1)} %get-tuple-element.85.refs_14_.refs_0_, bf16[256,1024]{1,0:T(8,128)(2,1)} %collective-permute-done.17.refs_1_, ...), custom_call_target="tpu_custom_call" | custom-call | flops 17179869184 | bytes 33554432 | tf_op jit(solution)/shard_map/outp/pallas_call | solution.py:461
  606.3 43.8 %flash.7 = (bf16[256,1024]{1,0:T(8,128)(2,1)}, bf16[256,1024]{1,0:T(8,128)(2,1)}, bf16[256,1024]{1,0:T(8,128)(2,1)}, bf16[256,1024]{1,0:T(8,128)(2,1)}) custom-call(s32[969]{0:T(1024)} %bitcast.32, bf16[8,1024,256]{2,1,0:T(8,128)(2,1)} %get-tuple-element.74.refs_1_, bf16[2,1024,256]{2,1,0:T(8,128)(2,1)} %get-tuple-element.102.refs_2_, ...), custom_call_target="tpu_custom_call" | custom-call | flops 32212254720 | bytes 8388608 | tf_op jit(solution)/shard_map/flash/pallas_call | solution.py:351
  658.7 88.2 %mlp.5 = (bf16[512,4096]{1,0:T(8,128)(2,1)}, bf16[512,4096]{1,0:T(8,128)(2,1)}) custom-call(bf16[256,4096]{1,0:T(8,128)(2,1)} %get-tuple-element.101.refs_0_, bf16[256,4096]{1,0:T(8,128)(2,1)} %collective-permute-done.32.refs_1_, bf16[256,4096]{1,0:T(8,128)(2,1)} %collective-permute-done.33.refs_2_, bf16[256,4096]{1,0:T(8,128)(2,1)} %collective-permute-done.34.refs_3_, ...), custom_call_target="tpu_custom_call" | custom-call | flops 77309411328 | bytes 75497472 | tf_op jit(solution)/shard_map/mlp/pallas_call | solution.py:551
  748.9 6.3 collective-permute-done.36.refs_1_
  755.3 7.2 collective-permute-done.37.refs_2_
  762.9 9.3 collective-permute-done.38.refs_3_
  773.6 11.4 collective-permute-done.40.refs_6_
  785.0 9.6 collective-permute-done.41.refs_7_
  794.6 29.0 %outp.3 = (bf16[256,4096]{1,0:T(8,128)(2,1)}, bf16[256,4096]{1,0:T(8,128)(2,1)}, bf16[256,4096]{1,0:T(8,128)(2,1)}, bf16[256,4096]{1,0:T(8,128)(2,1)}) custom-call(bf16[256,1024]{1,0:T(8,128)(2,1)} %get-tuple-element.99.refs_20_.refs_0_, bf16[256,1024]{1,0:T(8,128)(2,1)} %collective-permute-done.36.refs_1_, ...), custom_call_target="tpu_custom_call" | custom-call | flops 17179869184 | bytes 33554432 | tf_op jit(solution)/shard_map/outp/pallas_call | solution.py:461
  828.0 88.4 %mlp.6 = (bf16[512,4096]{1,0:T(8,128)(2,1)}, bf16[512,4096]{1,0:T(8,128)(2,1)}) custom-call(bf16[256,4096]{1,0:T(8,128)(2,1)} %get-tuple-element.117.refs_0_, bf16[256,4096]{1,0:T(8,128)(2,1)} %collective-permute-done.44.refs_1_, bf16[256,4096]{1,0:T(8,128)(2,1)} %collective-permute-done.45.refs_2_, bf16[256,4096]{1,0:T(8,128)(2,1)} %collective-permute-done.46.refs_3_, ...), custom_call_target="tpu_custom_call" | custom-call | flops 77309411328 | bytes 75497472 | tf_op jit(solution)/shard_map/mlp/pallas_call | solution.py:551
  917.4 47.5 %collective-permute-done.43.refs_1_ = bf16[256,4096]{1,0:T(8,128)(2,1)S(1)} collective-permute-done((bf16[256,4096]{1,0:T(8,128)(2,1)}, bf16[256,4096]{1,0:T(8,128)(2,1)S(1)}, u32[]{:S(2)}, u32[]{:S(2)}) %collective-permute-start.43) | collective-permute-done | bytes 2097184 | tf_op jit(solution)/shard_map/ppermute | solution.py:692
  964.9 5.3 add_convert_fusion.1.refs_7_
  971.5 88.3 %mlp.7 = (bf16[512,4096]{1,0:T(8,128)(2,1)}, bf16[512,4096]{1,0:T(8,128)(2,1)}) custom-call(bf16[256,4096]{1,0:T(8,128)(2,1)} %get-tuple-element.116.refs_0_, bf16[256,4096]{1,0:T(8,128)(2,1)} %copy-done.3, bf16[256,4096]{1,0:T(8,128)(2,1)} %copy-done.4, bf16[256,4096]{1,0:T(8,128)(2,1)} %collective-permute-done.48.refs_3_, bf16[4096,3072]{1,0:T(8,128)(2,1)} %refs_4_.9, ...), custom_call_target="tpu_custom_call" | custom-call | flops 77309411328 | bytes 75497472 | tf_op jit(solution)/shard_map/mlp/pallas_call | solution.py:551
  1062.3 46.8 %collective-permute-done.51.refs_1_ = bf16[256,4096]{1,0:T(8,128)(2,1)} collective-permute-done((bf16[256,4096]{1,0:T(8,128)(2,1)}, bf16[256,4096]{1,0:T(8,128)(2,1)}, u32[]{:S(2)}, u32[]{:S(2)}) %collective-permute-start.51) | collective-permute-done | bytes 2097184 | tf_op jit(solution)/shard_map/ppermute | solution.py:692
  1109.4 44.7 %collective-permute-done.42.refs_2_ = bf16[256,4096]{1,0:T(8,128)(2,1)} collective-permute-done((bf16[256,4096]{1,0:T(8,128)(2,1)}, bf16[256,4096]{1,0:T(8,128)(2,1)}, u32[]{:S(2)}, u32[]{:S(2)}) %collective-permute-start.42) | collective-permute-done | bytes 2097184 | tf_op jit(solution)/shard_map/ppermute | solution.py:692
  1154.0 5.8 zsum.5.refs_0_
  1164.2 49.6 %mlp.8 = (bf16[256,4096]{1,0:T(8,128)(2,1)}, bf16[256,4096]{1,0:T(8,128)(2,1)}) custom-call(bf16[256,4096]{1,0:T(8,128)(2,1)} %get-tuple-element.124.refs_0_, bf16[256,4096]{1,0:T(8,128)(2,1)} %collective-permute-done.51.refs_1_, bf16[256,4096]{1,0:T(8,128)(2,1)} %collective-permute-done.52.refs_2_, bf16[256,4096]{1,0:T(8,128)(2,1)} %collective-permute-done.53.refs_3_, ...), custom_call_target="tpu_custom_call" | custom-call | flops 38654705664 | bytes 75497472 | tf_op jit(solution)/shard_map/mlp/pallas_call | solution.py:551
  1214.1 5.6 zsum.6.refs_0_
  1222.5 49.5 %mlp.9 = (bf16[256,4096]{1,0:T(8,128)(2,1)}, bf16[256,4096]{1,0:T(8,128)(2,1)}) custom-call(bf16[256,4096]{1,0:T(8,128)(2,1)} %get-tuple-element.124.refs_0_, bf16[256,4096]{1,0:T(8,128)(2,1)} %collective-permute-done.51.refs_1_, bf16[256,4096]{1,0:T(8,128)(2,1)} %collective-permute-done.52.refs_2_, bf16[256,4096]{1,0:T(8,128)(2,1)} %collective-permute-done.53.refs_3_, ...), custom_call_target="tpu_custom_call" | custom-call | flops 38654705664 | bytes 75497472 | tf_op jit(solution)/shard_map/mlp/pallas_call | solution.py:551
  1273.9 5.6 zsum.7.refs_0_
  1282.6 16.0 %collective-permute-done.57.refs_3_ = bf16[128,4096]{1,0:T(8,128)(2,1)} collective-permute-done((bf16[128,4096]{1,0:T(8,128)(2,1)}, bf16[128,4096]{1,0:T(8,128)(2,1)}, u32[]{:S(2)}, u32[]{:S(2)}) %collective-permute-start.57) | collective-permute-done | bytes 1048608 | tf_op jit(solution)/shard_map/ppermute | solution.py:692
  1301.8 18.6 %collective-permute-done.59.refs_3_ = bf16[128,4096]{1,0:T(8,128)(2,1)} collective-permute-done((bf16[128,4096]{1,0:T(8,128)(2,1)}, bf16[128,4096]{1,0:T(8,128)(2,1)}, u32[]{:S(2)}, u32[]{:S(2)}) %collective-permute-start.59) | collective-permute-done | bytes 1048608 | tf_op jit(solution)/shard_map/ppermute | solution.py:692
  (124 shorter events, 100.7 us)
Async XLA Ops:
  4.7 73.1 %collective-permute-start.4 = (bf16[256,4096]{1,0:T(8,128)(2,1)}, bf16[256,4096]{1,0:T(8,128)(2,1)}, u32[]{:S(2)}, u32[]{:S(2)}) collective-permute-start(bf16[256,4096]{1,0:T(8,128)(2,1)} %norm.4.refs_2_.refs_0_), channel_id=1, source_target_pairs={{0,2},{1,3},{2,0},{3,1},{4,6},{5,7},{6,4},{7,5}} | collective-permute-start | bytes 6291464 | tf_op jit(solution)/shard_map/ppermute | solution.py:692
  8.0 30.0 %collective-permute-start = (bf16[256,4096]{1,0:T(8,128)(2,1)}, bf16[256,4096]{1,0:T(8,128)(2,1)}, u32[]{:S(2)}, u32[]{:S(2)}) collective-permute-start(bf16[256,4096]{1,0:T(8,128)(2,1)} %norm.4.refs_2_.refs_0_), channel_id=1, source_target_pairs={{0,1},{1,0},{2,3},{3,2},{4,5},{5,4},{6,7},{7,6}} | collective-permute-start | bytes 6291464 | tf_op jit(solution)/shard_map/ppermute | solution.py:692
  11.4 26.6 %collective-permute-start.1 = (bf16[256,4096]{1,0:T(8,128)(2,1)}, bf16[256,4096]{1,0:T(8,128)(2,1)}, u32[]{:S(2)}, u32[]{:S(2)}) collective-permute-start(bf16[256,4096]{1,0:T(8,128)(2,1)} %norm.5.refs_2_.refs_1_), channel_id=1, source_target_pairs={{0,1},{1,0},{2,3},{3,2},{4,5},{5,4},{6,7},{7,6}} | collective-permute-start | bytes 6291464 | tf_op jit(solution)/shard_map/ppermute | solution.py:692
  15.3 22.7 %collective-permute-start.2 = (bf16[256,4096]{1,0:T(8,128)(2,1)}, bf16[256,4096]{1,0:T(8,128)(2,1)}, u32[]{:S(2)}, u32[]{:S(2)}) collective-permute-start(bf16[256,4096]{1,0:T(8,128)(2,1)} %norm.6.refs_2_), channel_id=1, source_target_pairs={{0,1},{1,0},{2,3},{3,2},{4,5},{5,4},{6,7},{7,6}} | collective-permute-start | bytes 6291464 | tf_op jit(solution)/shard_map/ppermute | solution.py:692
  18.8 19.2 %collective-permute-start.3 = (bf16[256,4096]{1,0:T(8,128)(2,1)}, bf16[256,4096]{1,0:T(8,128)(2,1)}, u32[]{:S(2)}, u32[]{:S(2)}) collective-permute-start(bf16[256,4096]{1,0:T(8,128)(2,1)} %norm.7.refs_3_), channel_id=1, source_target_pairs={{0,1},{1,0},{2,3},{3,2},{4,5},{5,4},{6,7},{7,6}} | collective-permute-start | bytes 6291464 | tf_op jit(solution)/shard_map/ppermute | solution.py:692
  77.8 48.3 %collective-permute-start.6 = (bf16[256,4096]{1,0:T(8,128)(2,1)}, bf16[256,4096]{1,0:T(8,128)(2,1)}, u32[]{:S(2)}, u32[]{:S(2)}) collective-permute-start(bf16[256,4096]{1,0:T(8,128)(2,1)} %norm.5.refs_2_.refs_1_), channel_id=1, source_target_pairs={{0,2},{1,3},{2,0},{3,1},{4,6},{5,7},{6,4},{7,5}} | collective-permute-start | bytes 6291464 | tf_op jit(solution)/shard_map/ppermute | solution.py:692
  126.2 71.7 %collective-permute-start.8 = (bf16[256,4096]{1,0:T(8,128)(2,1)}, bf16[256,4096]{1,0:T(8,128)(2,1)}, u32[]{:S(2)}, u32[]{:S(2)}) collective-permute-start(bf16[256,4096]{1,0:T(8,128)(2,1)} %norm.6.refs_2_), channel_id=1, source_target_pairs={{0,2},{1,3},{2,0},{3,1},{4,6},{5,7},{6,4},{7,5}} | collective-permute-start | bytes 6291464 | tf_op jit(solution)/shard_map/ppermute | solution.py:692
  199.7 47.9 %collective-permute-start.10 = (bf16[256,4096]{1,0:T(8,128)(2,1)}, bf16[256,4096]{1,0:T(8,128)(2,1)}, u32[]{:S(2)}, u32[]{:S(2)}) collective-permute-start(bf16[256,4096]{1,0:T(8,128)(2,1)} %norm.7.refs_3_), channel_id=1, source_target_pairs={{0,2},{1,3},{2,0},{3,1},{4,6},{5,7},{6,4},{7,5}} | collective-permute-start | bytes 6291464 | tf_op jit(solution)/shard_map/ppermute | solution.py:692
  247.6 48.8 %collective-permute-start.12 = (bf16[8,2,256,256]{3,2,1,0:T(8,128)(2,1)}, bf16[8,2,256,256]{3,2,1,0:T(8,128)(2,1)}, u32[]{:S(2)}, u32[]{:S(2)}) collective-permute-start(bf16[8,2,256,256]{3,2,1,0:T(8,128)(2,1)} %get-tuple-element.75.refs_5_.refs_3_), channel_id=1, source_target_pairs={{0,4},{4,0},{1,5},{5,1},{2,6},{6,2},{3,7},{7,3}} | collective-permute-start | bytes 6291464 | tf_op jit(solution)/shard_map/ppermute | solution.py:692
  249.1 58.5 %collective-permute-start.13 = (bf16[2,2,256,256]{3,2,1,0:T(8,128)(2,1)}, bf16[2,2,256,256]{3,2,1,0:T(8,128)(2,1)}, u32[]{:S(2)}, u32[]{:S(2)}) collective-permute-start(bf16[2,2,256,256]{3,2,1,0:T(8,128)(2,1)} %get-tuple-element.78.refs_5_.refs_4_), channel_id=1, source_target_pairs={{0,4},{4,0},{1,5},{5,1},{2,6},{6,2},{3,7},{7,3}} | collective-permute-start | bytes 1572872 | tf_op jit(solution)/shard_map/ppermute | solution.py:692
  249.6 69.3 %collective-permute-start.14 = (bf16[2,2,256,256]{3,2,1,0:T(8,128)(2,1)}, bf16[2,2,256,256]{3,2,1,0:T(8,128)(2,1)}, u32[]{:S(2)}, u32[]{:S(2)}) collective-permute-start(bf16[2,2,256,256]{3,2,1,0:T(8,128)(2,1)} %get-tuple-element.80.refs_5_), channel_id=1, source_target_pairs={{0,4},{4,0},{1,5},{5,1},{2,6},{6,2},{3,7},{7,3}} | collective-permute-start | bytes 1572872 | tf_op jit(solution)/shard_map/ppermute | solution.py:692
  251.1 79.0 %collective-permute-start.15 = (bf16[2,2,256,256]{3,2,1,0:T(8,128)(2,1)}, bf16[2,2,256,256]{3,2,1,0:T(8,128)(2,1)}, u32[]{:S(2)}, u32[]{:S(2)}) collective-permute-start(bf16[2,2,256,256]{3,2,1,0:T(8,128)(2,1)} %get-tuple-element.82.refs_5_.refs_6_), channel_id=1, source_target_pairs={{0,4},{4,0},{1,5},{5,1},{2,6},{6,2},{3,7},{7,3}} | collective-permute-start | bytes 1572872 | tf_op jit(solution)/shard_map/ppermute | solution.py:692
  266.2 74.7 %collective-permute-start.16 = (bf16[2,2,256,256]{3,2,1,0:T(8,128)(2,1)}, bf16[2,2,256,256]{3,2,1,0:T(8,128)(2,1)}, u32[]{:S(2)}, u32[]{:S(2)}) collective-permute-start(bf16[2,2,256,256]{3,2,1,0:T(8,128)(2,1)} %get-tuple-element.84.refs_7_.refs_14_), channel_id=1, source_target_pairs={{0,4},{4,0},{1,5},{5,1},{2,6},{6,2},{3,7},{7,3}} | collective-permute-start | bytes 1572872 | tf_op jit(solution)/shard_map/ppermute | solution.py:692
  296.4 274.4 %collective-permute-start.23 = (bf16[1024,4096]{1,0:T(8,128)(2,1)}, bf16[1024,4096]{1,0:T(8,128)(2,1)}, u32[]{:S(2)}, u32[]{:S(2)}) collective-permute-start(bf16[1024,4096]{1,0:T(8,128)(2,1)} %bitcast.23), channel_id=1, source_target_pairs={{0,1},{1,0},{2,3},{3,2},{4,5},{5,4},{6,7},{7,6}} | collective-permute-start | bytes 25165832 | tf_op jit(solution)/shard_map/ppermute | solution.py:692
  307.6 107.1 %collective-permute-start.25 = (bf16[256,4096]{1,0:T(8,128)(2,1)}, bf16[256,4096]{1,0:T(8,128)(2,1)}, u32[]{:S(2)}, u32[]{:S(2)}) collective-permute-start(bf16[256,4096]{1,0:T(8,128)(2,1)} %get-tuple-element.135), channel_id=1, source_target_pairs={{0,2},{1,3},{2,0},{3,1},{4,6},{5,7},{6,4},{7,5}} | collective-permute-start | bytes 6291464 | tf_op jit(solution)/shard_map/ppermute | solution.py:692
  318.9 95.9 %collective-permute-start.24 = (bf16[256,4096]{1,0:T(8,128)(2,1)}, bf16[256,4096]{1,0:T(8,128)(2,1)}, u32[]{:S(2)}, u32[]{:S(2)}) collective-permute-start(bf16[256,4096]{1,0:T(8,128)(2,1)} %get-tuple-element.136), channel_id=1, source_target_pairs={{0,2},{1,3},{2,0},{3,1},{4,6},{5,7},{6,4},{7,5}} | collective-permute-start | bytes 6291464 | tf_op jit(solution)/shard_map/ppermute | solution.py:692
  414.8 48.8 %collective-permute-start.27 = (bf16[256,4096]{1,0:T(8,128)(2,1)}, bf16[256,4096]{1,0:T(8,128)(2,1)}, u32[]{:S(2)}, u32[]{:S(2)}) collective-permute-start(bf16[256,4096]{1,0:T(8,128)(2,1)} %collective-permute-done.25.refs_11_), channel_id=1, source_target_pairs={{0,4},{4,0},{1,5},{5,1},{2,6},{6,2},{3,7},{7,3}} | collective-permute-start | bytes 6291464 | tf_op jit(solution)/shard_map/ppermute | solution.py:692
  414.8 92.4 %collective-permute-start.26 = (bf16[256,4096]{1,0:T(8,128)(2,1)}, bf16[256,4096]{1,0:T(8,128)(2,1)}, u32[]{:S(2)}, u32[]{:S(2)}) collective-permute-start(bf16[256,4096]{1,0:T(8,128)(2,1)} %collective-permute-done.24.refs_10_), channel_id=1, source_target_pairs={{0,4},{4,0},{1,5},{5,1},{2,6},{6,2},{3,7},{7,3}} | collective-permute-start | bytes 6291464 | tf_op jit(solution)/shard_map/ppermute | solution.py:692
  416.8 11.5 collective-permute-start.17
  416.8 24.6 %collective-permute-start.18 = (bf16[256,1024]{1,0:T(8,128)(2,1)}, bf16[256,1024]{1,0:T(8,128)(2,1)}, u32[]{:S(2)}, u32[]{:S(2)}) collective-permute-start(bf16[256,1024]{1,0:T(8,128)(2,1)} %get-tuple-element.87), channel_id=1, source_target_pairs={{0,2},{1,3},{2,0},{3,1},{4,6},{5,7},{6,4},{7,5}} | collective-permute-start | bytes 1572872 | tf_op jit(solution)/shard_map/ppermute | solution.py:692
  428.3 134.3 %collective-permute-start.19 = (bf16[256,1024]{1,0:T(8,128)(2,1)}, bf16[256,1024]{1,0:T(8,128)(2,1)}, u32[]{:S(2)}, u32[]{:S(2)}) collective-permute-start(bf16[256,1024]{1,0:T(8,128)(2,1)} %get-tuple-element.88), channel_id=1, source_target_pairs={{0,3},{1,2},{2,1},{3,0},{4,7},{5,6},{6,5},{7,4}} | collective-permute-start | bytes 1572872 | tf_op jit(solution)/shard_map/ppermute | solution.py:692
  441.4 122.3 %collective-permute-start.20 = (bf16[256,1024]{1,0:T(8,128)(2,1)}, bf16[256,1024]{1,0:T(8,128)(2,1)}, u32[]{:S(2)}, u32[]{:S(2)}) collective-permute-start(bf16[256,1024]{1,0:T(8,128)(2,1)} %get-tuple-element.91), channel_id=1, source_target_pairs={{0,1},{1,0},{2,3},{3,2},{4,5},{5,4},{6,7},{7,6}} | collective-permute-start | bytes 1572872 | tf_op jit(solution)/shard_map/ppermute | solution.py:692
  463.6 100.1 %collective-permute-start.21 = (bf16[256,1024]{1,0:T(8,128)(2,1)}, bf16[256,1024]{1,0:T(8,128)(2,1)}, u32[]{:S(2)}, u32[]{:S(2)}) collective-permute-start(bf16[256,1024]{1,0:T(8,128)(2,1)} %get-tuple-element.92), channel_id=1, source_target_pairs={{0,2},{1,3},{2,0},{3,1},{4,6},{5,7},{6,4},{7,5}} | collective-permute-start | bytes 1572872 | tf_op jit(solution)/shard_map/ppermute | solution.py:692
  507.2 57.0 %collective-permute-start.22 = (bf16[256,1024]{1,0:T(8,128)(2,1)}, bf16[256,1024]{1,0:T(8,128)(2,1)}, u32[]{:S(2)}, u32[]{:S(2)}) collective-permute-start(bf16[256,1024]{1,0:T(8,128)(2,1)} %get-tuple-element.93), channel_id=1, source_target_pairs={{0,3},{1,2},{2,1},{3,0},{4,7},{5,6},{6,5},{7,4}} | collective-permute-start | bytes 1572872 | tf_op jit(solution)/shard_map/ppermute | solution.py:692
  564.2 12.6 collective-permute-start.30
  605.9 48.7 %collective-permute-start.33 = (bf16[256,4096]{1,0:T(8,128)(2,1)}, bf16[256,4096]{1,0:T(8,128)(2,1)}, u32[]{:S(2)}, u32[]{:S(2)}) collective-permute-start(bf16[256,4096]{1,0:T(8,128)(2,1)} %get-tuple-element.101.refs_0_), channel_id=1, source_target_pairs={{0,1},{1,0},{2,3},{3,2},{4,5},{5,4},{6,7},{7,6}} | collective-permute-start | bytes 6291464 | tf_op jit(solution)/shard_map/ppermute | solution.py:692
  606.2 48.0 %collective-permute-start.32 = (bf16[256,4096]{1,0:T(8,128)(2,1)}, bf16[256,4096]{1,0:T(8,128)(2,1)}, u32[]{:S(2)}, u32[]{:S(2)}) collective-permute-start(bf16[256,4096]{1,0:T(8,128)(2,1)} %get-tuple-element.101.refs_0_), channel_id=1, source_target_pairs={{0,2},{1,3},{2,0},{3,1},{4,6},{5,7},{6,4},{7,5}} | collective-permute-start | bytes 6291464 | tf_op jit(solution)/shard_map/ppermute | solution.py:692
  654.2 108.6 %collective-permute-start.44 = (bf16[256,4096]{1,0:T(8,128)(2,1)}, bf16[256,4096]{1,0:T(8,128)(2,1)}, u32[]{:S(2)}, u32[]{:S(2)}) collective-permute-start(bf16[256,4096]{1,0:T(8,128)(2,1)} %get-tuple-element.117.refs_0_), channel_id=1, source_target_pairs={{0,2},{1,3},{2,0},{3,1},{4,6},{5,7},{6,4},{7,5}} | collective-permute-start | bytes 6291464 | tf_op jit(solution)/shard_map/ppermute | solution.py:692
  746.9 76.7 %collective-permute-start.35 = (bf16[512,4096]{1,0:T(8,128)(2,1)}, bf16[512,4096]{1,0:T(8,128)(2,1)}, u32[]{:S(2)}, u32[]{:S(2)}) collective-permute-start(bf16[512,4096]{1,0:T(8,128)(2,1)} %get-tuple-element.107), channel_id=1, source_target_pairs={{0,1},{1,0},{2,3},{3,2},{4,5},{5,4},{6,7},{7,6}} | collective-permute-start | bytes 12582920 | tf_op jit(solution)/shard_map/ppermute | solution.py:692
  747.5 15.1 %collective-permute-start.37 = (bf16[256,1024]{1,0:T(8,128)(2,1)}, bf16[256,1024]{1,0:T(8,128)(2,1)}, u32[]{:S(2)}, u32[]{:S(2)}) collective-permute-start(bf16[256,1024]{1,0:T(8,128)(2,1)} %get-tuple-element.109), channel_id=1, source_target_pairs={{0,2},{1,3},{2,0},{3,1},{4,6},{5,7},{6,4},{7,5}} | collective-permute-start | bytes 1572872 | tf_op jit(solution)/shard_map/ppermute | solution.py:692
  747.7 24.4 %collective-permute-start.38 = (bf16[256,1024]{1,0:T(8,128)(2,1)}, bf16[256,1024]{1,0:T(8,128)(2,1)}, u32[]{:S(2)}, u32[]{:S(2)}) collective-permute-start(bf16[256,1024]{1,0:T(8,128)(2,1)} %get-tuple-element.110), channel_id=1, source_target_pairs={{0,3},{1,2},{2,1},{3,0},{4,7},{5,6},{6,5},{7,4}} | collective-permute-start | bytes 1572872 | tf_op jit(solution)/shard_map/ppermute | solution.py:692
  755.2 18.4 %collective-permute-start.39 = (bf16[256,1024]{1,0:T(8,128)(2,1)}, bf16[256,1024]{1,0:T(8,128)(2,1)}, u32[]{:S(2)}, u32[]{:S(2)}) collective-permute-start(bf16[256,1024]{1,0:T(8,128)(2,1)} %get-tuple-element.111), channel_id=1, source_target_pairs={{0,1},{1,0},{2,3},{3,2},{4,5},{5,4},{6,7},{7,6}} | collective-permute-start | bytes 1572872 | tf_op jit(solution)/shard_map/ppermute | solution.py:692
  762.6 22.5 %collective-permute-start.40 = (bf16[256,1024]{1,0:T(8,128)(2,1)}, bf16[256,1024]{1,0:T(8,128)(2,1)}, u32[]{:S(2)}, u32[]{:S(2)}) collective-permute-start(bf16[256,1024]{1,0:T(8,128)(2,1)} %get-tuple-element.112), channel_id=1, source_target_pairs={{0,2},{1,3},{2,0},{3,1},{4,6},{5,7},{6,4},{7,5}} | collective-permute-start | bytes 1572872 | tf_op jit(solution)/shard_map/ppermute | solution.py:692
  762.9 31.7 %collective-permute-start.41 = (bf16[256,1024]{1,0:T(8,128)(2,1)}, bf16[256,1024]{1,0:T(8,128)(2,1)}, u32[]{:S(2)}, u32[]{:S(2)}) collective-permute-start(bf16[256,1024]{1,0:T(8,128)(2,1)} %get-tuple-element.113), channel_id=1, source_target_pairs={{0,3},{1,2},{2,1},{3,0},{4,7},{5,6},{6,5},{7,4}} | collective-permute-start | bytes 1572872 | tf_op jit(solution)/shard_map/ppermute | solution.py:692
  772.1 55.8 %collective-permute-start.45 = (bf16[256,4096]{1,0:T(8,128)(2,1)}, bf16[256,4096]{1,0:T(8,128)(2,1)}, u32[]{:S(2)}, u32[]{:S(2)}) collective-permute-start(bf16[256,4096]{1,0:T(8,128)(2,1)} %get-tuple-element.117.refs_0_), channel_id=1, source_target_pairs={{0,1},{1,0},{2,3},{3,2},{4,5},{5,4},{6,7},{7,6}} | collective-permute-start | bytes 6291464 | tf_op jit(solution)/shard_map/ppermute | solution.py:692
  773.6 54.3 %collective-permute-start.46 = (bf16[256,4096]{1,0:T(8,128)(2,1)}, bf16[256,4096]{1,0:T(8,128)(2,1)}, u32[]{:S(2)}, u32[]{:S(2)}) collective-permute-start(bf16[256,4096]{1,0:T(8,128)(2,1)} %collective-permute-done.44.refs_1_), channel_id=1, source_target_pairs={{0,1},{1,0},{2,3},{3,2},{4,5},{5,4},{6,7},{7,6}} | collective-permute-start | bytes 6291464 | tf_op jit(solution)/shard_map/ppermute | solution.py:692
  916.4 48.5 %collective-permute-start.49 = (bf16[512,4096]{1,0:T(8,128)(2,1)}, bf16[512,4096]{1,0:T(8,128)(2,1)S(1)}, u32[]{:S(2)}, u32[]{:S(2)}) collective-permute-start(bf16[512,4096]{1,0:T(8,128)(2,1)} %get-tuple-element.121), channel_id=1, source_target_pairs={{0,1},{1,0},{2,3},{3,2},{4,5},{5,4},{6,7},{7,6}} | collective-permute-start | bytes 12582920 | tf_op jit(solution)/shard_map/ppermute | solution.py:692
  917.1 47.8 %collective-permute-start.43 = (bf16[256,4096]{1,0:T(8,128)(2,1)}, bf16[256,4096]{1,0:T(8,128)(2,1)S(1)}, u32[]{:S(2)}, u32[]{:S(2)}) collective-permute-start(bf16[256,4096]{1,0:T(8,128)(2,1)} %get-tuple-element.116.refs_0_), channel_id=1, source_target_pairs={{0,2},{1,3},{2,0},{3,1},{4,6},{5,7},{6,4},{7,5}} | collective-permute-start | bytes 6291464 | tf_op jit(solution)/shard_map/ppermute | solution.py:692
  917.4 52.8 %collective-permute-start.47 = (bf16[256,4096]{1,0:T(8,128)(2,1)}, bf16[256,4096]{1,0:T(8,128)(2,1)S(1)}, u32[]{:S(2)}, u32[]{:S(2)}) collective-permute-start(bf16[256,4096]{1,0:T(8,128)(2,1)} %get-tuple-element.116.refs_0_), channel_id=1, source_target_pairs={{0,1},{1,0},{2,3},{3,2},{4,5},{5,4},{6,7},{7,6}} | collective-permute-start | bytes 6291464 | tf_op jit(solution)/shard_map/ppermute | solution.py:692
  1059.8 100.0 %collective-permute-start.54 = (bf16[512,4096]{1,0:T(8,128)(2,1)}, bf16[512,4096]{1,0:T(8,128)(2,1)}, u32[]{:S(2)}, u32[]{:S(2)}) collective-permute-start(bf16[512,4096]{1,0:T(8,128)(2,1)} %get-tuple-element.127), channel_id=1, source_target_pairs={{0,1},{1,0},{2,3},{3,2},{4,5},{5,4},{6,7},{7,6}} | collective-permute-start | bytes 12582920 | tf_op jit(solution)/shard_map/ppermute | solution.py:692
  1060.3 48.8 %collective-permute-start.51 = (bf16[256,4096]{1,0:T(8,128)(2,1)}, bf16[256,4096]{1,0:T(8,128)(2,1)}, u32[]{:S(2)}, u32[]{:S(2)}) collective-permute-start(bf16[256,4096]{1,0:T(8,128)(2,1)} %get-tuple-element.124.refs_0_), channel_id=1, source_target_pairs={{0,2},{1,3},{2,0},{3,1},{4,6},{5,7},{6,4},{7,5}} | collective-permute-start | bytes 6291464 | tf_op jit(solution)/shard_map/ppermute | solution.py:692
  1060.5 93.5 %collective-permute-start.42 = (bf16[256,4096]{1,0:T(8,128)(2,1)}, bf16[256,4096]{1,0:T(8,128)(2,1)}, u32[]{:S(2)}, u32[]{:S(2)}) collective-permute-start(bf16[256,4096]{1,0:T(8,128)(2,1)} %add_convert_fusion.2.refs_7_), channel_id=1, source_target_pairs={{0,2},{1,3},{2,0},{3,1},{4,6},{5,7},{6,4},{7,5}} | collective-permute-start | bytes 6291464 | tf_op jit(solution)/shard_map/ppermute | solution.py:692
  1062.3 101.9 %collective-permute-start.52 = (bf16[256,4096]{1,0:T(8,128)(2,1)}, bf16[256,4096]{1,0:T(8,128)(2,1)}, u32[]{:S(2)}, u32[]{:S(2)}) collective-permute-start(bf16[256,4096]{1,0:T(8,128)(2,1)} %get-tuple-element.124.refs_0_), channel_id=1, source_target_pairs={{0,1},{1,0},{2,3},{3,2},{4,5},{5,4},{6,7},{7,6}} | collective-permute-start | bytes 6291464 | tf_op jit(solution)/shard_map/ppermute | solution.py:692
  1109.1 55.1 %collective-permute-start.53 = (bf16[256,4096]{1,0:T(8,128)(2,1)}, bf16[256,4096]{1,0:T(8,128)(2,1)}, u32[]{:S(2)}, u32[]{:S(2)}) collective-permute-start(bf16[256,4096]{1,0:T(8,128)(2,1)} %collective-permute-done.51.refs_1_), channel_id=1, source_target_pairs={{0,1},{1,0},{2,3},{3,2},{4,5},{5,4},{6,7},{7,6}} | collective-permute-start | bytes 6291464 | tf_op jit(solution)/shard_map/ppermute | solution.py:692
  1109.1 105.0 %collective-permute-start.50 = (bf16[256,4096]{1,0:T(8,128)(2,1)}, bf16[256,4096]{1,0:T(8,128)(2,1)}, u32[]{:S(2)}, u32[]{:S(2)}) collective-permute-start(bf16[256,4096]{1,0:T(8,128)(2,1)} %add_convert_fusion.1.refs_7_), channel_id=1, source_target_pairs={{0,2},{1,3},{2,0},{3,1},{4,6},{5,7},{6,4},{7,5}} | collective-permute-start | bytes 6291464 | tf_op jit(solution)/shard_map/ppermute | solution.py:692
  1213.8 60.1 %collective-permute-start.55 = (bf16[256,4096]{1,0:T(8,128)(2,1)}, bf16[256,4096]{1,0:T(8,128)(2,1)}, u32[]{:S(2)}, u32[]{:S(2)}) collective-permute-start(bf16[256,4096]{1,0:T(8,128)(2,1)} %add_convert_fusion.refs_7_), channel_id=1, source_target_pairs={{0,2},{1,3},{2,0},{3,1},{4,6},{5,7},{6,4},{7,5}} | collective-permute-start | bytes 6291464 | tf_op jit(solution)/shard_map/ppermute | solution.py:692
  1272.2 26.3 %collective-permute-start.57 = (bf16[128,4096]{1,0:T(8,128)(2,1)}, bf16[128,4096]{1,0:T(8,128)(2,1)}, u32[]{:S(2)}, u32[]{:S(2)}) collective-permute-start(bf16[128,4096]{1,0:T(8,128)(2,1)} %add_convert_fusion.4.refs_7_), channel_id=1, source_target_pairs={{0,2},{1,3},{2,0},{3,1},{4,6},{5,7},{6,4},{7,5}} | collective-permute-start | bytes 3145736 | tf_op jit(solution)/shard_map/ppermute | solution.py:692
  1282.3 38.1 %collective-permute-start.59 = (bf16[128,4096]{1,0:T(8,128)(2,1)}, bf16[128,4096]{1,0:T(8,128)(2,1)}, u32[]{:S(2)}, u32[]{:S(2)}) collective-permute-start(bf16[128,4096]{1,0:T(8,128)(2,1)} %add_convert_fusion.3.refs_5_), channel_id=1, source_target_pairs={{0,2},{1,3},{2,0},{3,1},{4,6},{5,7},{6,4},{7,5}} | collective-permute-start | bytes 3145736 | tf_op jit(solution)/shard_map/ppermute | solution.py:692
  (17 other events, 93.4 us)

commit v8 on v7

--- a/solution.py
+++ b/solution.py
@@ -66,13 +66,14 @@
     )(x_rows, gain, *after)
 
 
-def qkv_kernel(*refs, n_in, n_q, group):
+def qkv_kernel(*refs, n_in, n_q, group, first, with_q, with_kv):
     a_refs = refs[:n_in]
-    w_ref, cos_ref, sin_ref, q_ref, kv_ref, a_scr, sem = refs[n_in:]
-    n = pl.program_id(0)
+    w_ref, cos_ref, sin_ref, *outs, a_scr, sem = refs[n_in:]
+    q_ref, kv_ref = outs[0], outs[-1]
+    n = pl.program_id(0) + first
     heads = w_ref.shape[1] // HD
 
-    @pl.when(n == 0)
+    @pl.when(n == first)
     def _():
         for k, r in enumerate(a_refs):
             pltpu.make_async_copy(r, a_scr.at[pl.ds(k * RUN, RUN), :], sem.at[k]).start()
@@ -83,7 +84,7 @@
         return jnp.concatenate([lo * cos - hi * sin, hi * cos + lo * sin], axis=0)
 
     def one(k, carry):
-        @pl.when(n == 0)
+        @pl.when(n == first)
         def _():
             for i in range(group):
                 rows = pl.ds(pl.multiple_of((k * group + i) * RUN, RUN), RUN)
@@ -95,13 +96,13 @@
         def piece(i, h):
             return r[i * RUN:(i + 1) * RUN, h * HD:(h + 1) * HD].T
 
-        @pl.when(n < n_q)
+        @pl.when((n < n_q) if with_q else False)
         def _():
             for i in range(group):
                 for h in range(heads):
                     q_ref[k * group + i, h * HD:(h + 1) * HD, :] = rope(piece(i, h), k * group + i).astype(BF)
 
-        @pl.when(n == n_q)
+        @pl.when((n == n_q) if with_kv else False)
         def _():
             for i in range(group):
                 for h in range(heads // 2):
@@ -113,21 +114,24 @@
     lax.fori_loop(0, n_in // group, one, 0)
 
 
-def qkv(rows, w_all, tables, after=(), group=2):
+def qkv(rows, w_all, tables, with_q=True, with_kv=True, after=(), group=2):
     n_in = len(rows)
     dim = w_all.shape[0]
     tn = 512
     n_q = w_all.shape[1] // tn - 1
     (cos, sin), first_run = tables
     at = first_run // n_in
+    start = 0 if with_q else n_q
+    kv_shape = (n_in, 2, RUN, RUN)
     tab = pl.BlockSpec((n_in, HD // 2, RUN), lambda n: (at, 0, 0))
     return pl.pallas_call(
-        ordered(functools.partial(qkv_kernel, n_in=n_in, n_q=n_q, group=group), n_in + 3, after),
-        grid=(n_q + 1,),
-        in_specs=[ANY] * n_in + [pl.BlockSpec((dim, tn), lambda n: (0, n)), tab, tab] + [ANY] * len(after),
-        out_specs=[pl.BlockSpec((n_in, tn, RUN), lambda n: (0, jnp.minimum(n, n_q - 1), 0)),
-                   pl.BlockSpec((n_in, 2, 256, 256), lambda n: (0, 0, 0, 0))],
-        out_shape=[jax.ShapeDtypeStruct((n_in, n_q * tn, RUN), BF), jax.ShapeDtypeStruct((n_in, 2, 256, 256), BF)],
+        ordered(functools.partial(qkv_kernel, n_in=n_in, n_q=n_q, group=group, first=start, with_q=with_q, with_kv=with_kv),
+                n_in + 3, after),
+        grid=(n_q * with_q + with_kv,),
+        in_specs=[ANY] * n_in + [pl.BlockSpec((dim, tn), lambda n: (0, n + start)), tab, tab] + [ANY] * len(after),
+        out_specs=[pl.BlockSpec((n_in, tn, RUN), lambda n: (0, jnp.minimum(n, n_q - 1), 0))] * with_q
+        + [pl.BlockSpec(kv_shape, lambda n: (0,) * len(kv_shape))] * with_kv,
+        out_shape=[jax.ShapeDtypeStruct((n_in, n_q * tn, RUN), BF)] * with_q + [jax.ShapeDtypeStruct(kv_shape, BF)] * with_kv,
         scratch_shapes=[pltpu.VMEM((n_in * RUN, dim), BF), pltpu.SemaphoreType.DMA((n_in,))],
         name="qkv", compiler_params=params(1),
         cost_estimate=cost(2 * n_in * RUN * w_all.size, 2 * w_all.size),
@@ -372,7 +376,7 @@
         out_shape=[jax.ShapeDtypeStruct((RUN, nq), BF)] * n_tiles if final
         else [jax.ShapeDtypeStruct((st_tiles, *state), F32)],
         input_output_aliases={n_in - 1: 0} if sts and not final else {},
-        name="flash" if final else "flash_part", compiler_params=pltpu.CompilerParams(vmem_limit_bytes=VMEM),
+        name="flash" if final else "flash_part", compiler_params=params(0),
         cost_estimate=cost(8 * work * RUN * RUN * nq, n_runs * RUN * nq),
     )(tab, *qs, *kvs, *sts, *after)
 
@@ -479,21 +483,16 @@
     i = pl.program_id(0)
 
     def fetch(j):
-        def tile(src, dst, sem):
-            part = src.shape[0] // 4
-            for r in range(0, src.shape[0], part):
-                pltpu.make_async_copy(src.at[pl.ds(r, part), :], dst.at[pl.ds(r, part), :], sem).start()
-
         @pl.when(j < nk)
         def _():
-            cols = pl.ds(pl.multiple_of(j * tn, tn), tn)
+            slot, cols = lax.rem(j, 2), pl.ds(pl.multiple_of(j * tn, tn), tn)
             for k, w in enumerate((wg_ref, wu_ref)):
-                tile(w.at[:, cols], w_scr.at[lax.rem(j, 2), k], w_sem.at[lax.rem(j, 2)])
+                pltpu.make_async_copy(w.at[:, cols], w_scr.at[slot, k], w_sem.at[slot]).start()
 
         @pl.when((j >= nk) & (j < nk + nd))
         def _():
-            n = j - nk
-            tile(wd_ref.at[:, pl.ds(pl.multiple_of(n * td, td), td)], d_scr.at[lax.rem(n, 2)], d_sem.at[lax.rem(n, 2)])
+            n, slot = j - nk, lax.rem(j - nk, 2)
+            pltpu.make_async_copy(wd_ref.at[:, pl.ds(pl.multiple_of(n * td, td), td)], d_scr.at[slot], d_sem.at[slot]).start()
 
     def gated(rows, cols, slot):
         b = b_scr[rows, :]
@@ -706,7 +705,12 @@
 
         def far_qkv(j, after):
             here = tied(far[j], after)
-            q, kv = qkv([here, send(over_core, here)], w_all, (tables, 2 * (n_run + j)), after=(after,))
+            rows = [here, send(over_core, here)], w_all, (tables, 2 * (n_run + j))
+            if j + 1 < n_run:
+                q, kv = qkv(*rows, after=(after,))
+            else:
+                kv, = qkv(*rows, False, after=(after,))
+                q, = qkv(*rows, True, False, after=(kv, gm))
             q_far.append(q)
             kvs.append(kv)
             return kv
@@ -728,7 +732,7 @@
         far_qkv(3, far_qkv(2, st))
         kvs = kvs + [send(over_y, kv) for kv in kvs]
 
-        os, outs, prev = [], [], kvs[n_run]
+        os, outs, prev = [], [], q_far[-1]
         wo_a, wo_ya, wo_yb = {}, {}, {}
 
         def forward_w(p):
@@ -794,8 +798,8 @@
                 relay_b(c + 1)
             if c == 0:
                 prev = project(1)
-            elif c > 1:
-                prev = z = finish(c - 2)
+            elif c < n_run:
+                prev = z = finish(c - 1)
             kept = keep if prev is keep else tied(keep, prev)
             prev = s_far = (kept[size:].astype(F32) + recv[size:].astype(F32)).astype(BF)
             sums.append((keep, recv, send(over_x, s_far)))

time: 1330 us -> 1370 us (1.030)
  waiting for transfers between devices: 441 us -> 483 us
    ppermute x60, waiting for transfers between devices: 441 us -> 483 us  [send(): return lax.ppermute(v, *axis_pairs)]
    pallas_call x5 -> x6, Pallas kernels: 96.4 us -> 101 us  [qkv(): pl.pallas_call(ordered(functools.partial(qkv_kernel, n_in=n_in, n_q=n_q,...]
  transfers between devices with their start and end apart: 60 -> 60, of which waited for: 30 -> 31; matrix products, arithmetic and copies ran while one was open for 3% -> 3% of each run, Pallas kernels for 42% -> 37%
where the time goes in v8:
time: 1370 us; the launch traced here: 1360 us
  Pallas kernels  768 us (56%)
  waiting for transfers between devices  483 us (35%)
  starting transfers between devices  65.4 us (5%)
  local copies, waits for them, and re-layouts  23.9 us (2%)
  other arithmetic  23.2 us (2%)
    ppermute x60, waiting for transfers between devices, send(): return lax.ppermute(v, *axis_pairs)  483 us
    pallas_call x5, Pallas kernels, mlp(): pl.pallas_call(ordered(functools.partial(mlp_kernel, n_in=len(bs), first=...  356 us
    pallas_call x5, Pallas kernels, flash(): pl.pallas_call(ordered(functools.partial(flash_kernel, q_src=q_src, kv_sr...  215 us
    pallas_call x6, Pallas kernels, qkv(): pl.pallas_call(ordered(functools.partial(qkv_kernel, n_in=n_in, n_q=n_q,...  101 us
    ppermute x60, starting transfers between devices, send(): return lax.ppermute(v, *axis_pairs)  65.4 us
    pallas_call x2, Pallas kernels, out_proj(): pl.pallas_call(ordered(functools.partial(out_kernel, blocks=blocks, n_w=l...  58 us
  transfers between devices with their start and end apart: 60, of which 31 were waited for; matrix products, arithmetic and copies ran while one was open for 3% of the time, Pallas kernels for 37%

profile of v8, /device:TPU:0, one launch (start us, length us, event | category | flops | bytes accessed | tf_op | source)
XLA Modules:
  0.0 1364.3 jit_solution(12573149528367214656)
XLA Ops:
  20.1 9.3 bitcast_dynamic-update-slice_fusion
  29.4 4.8 multiply_sine_fusion
  38.1 39.7 %qkv.6 = (bf16[8,1024,256]{2,1,0:T(8,128)(2,1)}, bf16[8,2,256,256]{3,2,1,0:T(8,128)(2,1)}) custom-call(bf16[256,4096]{1,0:T(8,128)(2,1)} %norm.4.refs_2_.refs_0_, bf16[256,4096]{1,0:T(8,128)(2,1)} %norm.5.refs_2_.refs_1_, bf16[256,4096]{1,0:T(8,128)(2,1)} %norm.6.refs_2_, bf16[256,4096]{1,0:T(8,128)(2,1)} %norm.7.refs_3_, ...), custom_call_target="tpu_custom_call" | custom-call | flops 25769803776 | bytes 12582912 | tf_op jit(solution)/shard_map/qkv/pallas_call | solution.py:127
  82.3 14.1 %qkv.7 = (bf16[2,1024,256]{2,1,0:T(8,128)(2,1)}, bf16[2,2,256,256]{3,2,1,0:T(8,128)(2,1)}) custom-call(bf16[256,4096]{1,0:T(8,128)(2,1)} %collective-permute-done.4.refs_0_, bf16[256,4096]{1,0:T(8,128)(2,1)} %collective-permute-done.5.refs_1_, bf16[4096,1536]{1,0:T(8,128)(2,1)} %bitcast_dynamic-update-slice_fusion.1.refs_8_.refs_2_, ...), custom_call_target="tpu_custom_call" | custom-call | flops 6442450944 | bytes 12582912 | tf_op jit(solution)/shard_map/qkv/pallas_call | solution.py:127
  96.4 29.7 %collective-permute-done.6.refs_0_ = bf16[256,4096]{1,0:T(8,128)(2,1)} collective-permute-done((bf16[256,4096]{1,0:T(8,128)(2,1)}, bf16[256,4096]{1,0:T(8,128)(2,1)}, u32[]{:S(2)}, u32[]{:S(2)}) %collective-permute-start.6) | collective-permute-done | bytes 2097184 | tf_op jit(solution)/shard_map/ppermute | solution.py:691
  130.6 14.4 %qkv.8 = (bf16[2,1024,256]{2,1,0:T(8,128)(2,1)}, bf16[2,2,256,256]{3,2,1,0:T(8,128)(2,1)}) custom-call(bf16[256,4096]{1,0:T(8,128)(2,1)} %collective-permute-done.6.refs_0_, bf16[256,4096]{1,0:T(8,128)(2,1)} %collective-permute-done.7.refs_1_, bf16[4096,1536]{1,0:T(8,128)(2,1)} %bitcast_dynamic-update-slice_fusion.1.refs_8_.refs_2_, ...), custom_call_target="tpu_custom_call" | custom-call | flops 6442450944 | bytes 12582912 | tf_op jit(solution)/shard_map/qkv/pallas_call | solution.py:127
  145.0 52.9 %flash_part.1.refs_5_.refs_13_ = f32[10,2,4,144,256]{4,3,2,1,0:T(8,128)} custom-call(s32[969]{0:T(1024)} %bitcast.28, bf16[8,1024,256]{2,1,0:T(8,128)(2,1)} %get-tuple-element.72.refs_1_, bf16[2,1024,256]{2,1,0:T(8,128)(2,1)} %get-tuple-element.75.refs_2_, bf16[8,2,256,256]{3,2,1,0:T(8,128)(2,1)} %get-tuple-element.73.refs_5_.refs_3_, ...), custom_call_target="tpu_custom_call" | custom-call | flops 38654705664 | bytes 2621440 | tf_op jit(solution)/shard_map/flash_part/pallas_call | solution.py:355
  203.9 14.1 %qkv.9 = (bf16[2,1024,256]{2,1,0:T(8,128)(2,1)}, bf16[2,2,256,256]{3,2,1,0:T(8,128)(2,1)}) custom-call(bf16[256,4096]{1,0:T(8,128)(2,1)} %collective-permute-done.8.refs_0_, bf16[256,4096]{1,0:T(8,128)(2,1)} %collective-permute-done.9.refs_1_, bf16[4096,1536]{1,0:T(8,128)(2,1)} %bitcast_dynamic-update-slice_fusion.1.refs_8_.refs_2_, ...), custom_call_target="tpu_custom_call" | custom-call | flops 6442450944 | bytes 12582912 | tf_op jit(solution)/shard_map/qkv/pallas_call | solution.py:127
  218.0 29.6 %collective-permute-done.10.refs_0_ = bf16[256,4096]{1,0:T(8,128)(2,1)} collective-permute-done((bf16[256,4096]{1,0:T(8,128)(2,1)}, bf16[256,4096]{1,0:T(8,128)(2,1)}, u32[]{:S(2)}, u32[]{:S(2)}) %collective-permute-start.10) | collective-permute-done | bytes 2097184 | tf_op jit(solution)/shard_map/ppermute | solution.py:691
  252.5 4.8 constant_dynamic-slice_fusion
  257.8 7.9 qkv.10.refs_5_.refs_7_
  267.2 11.1 qkv.11.refs_14_.refs_2_
  278.3 18.1 %collective-permute-done.12.refs_8_ = bf16[8,2,256,256]{3,2,1,0:T(8,128)(2,1)} collective-permute-done((bf16[8,2,256,256]{3,2,1,0:T(8,128)(2,1)}, bf16[8,2,256,256]{3,2,1,0:T(8,128)(2,1)}, u32[]{:S(2)}, u32[]{:S(2)}) %collective-permute-start.12) | collective-permute-done | bytes 2097184 | tf_op jit(solution)/shard_map/ppermute | solution.py:691
  296.4 11.2 collective-permute-done.13.refs_9_
  308.0 10.9 collective-permute-done.14.refs_10_
  319.2 10.9 collective-permute-done.15.refs_11_
  330.1 10.8 collective-permute-done.16.refs_12_
  340.9 29.3 %flash.4 = (bf16[256,1024]{1,0:T(8,128)(2,1)}, bf16[256,1024]{1,0:T(8,128)(2,1)}, bf16[256,1024]{1,0:T(8,128)(2,1)}, bf16[256,1024]{1,0:T(8,128)(2,1)}) custom-call(s32[969]{0:T(1024)} %bitcast.29, bf16[8,1024,256]{2,1,0:T(8,128)(2,1)} %get-tuple-element.72.refs_1_, bf16[2,1024,256]{2,1,0:T(8,128)(2,1)} %get-tuple-element.75.refs_2_, ...), custom_call_target="tpu_custom_call" | custom-call | flops 27917287424 | bytes 8388608 | tf_op jit(solution)/shard_map/flash/pallas_call | solution.py:355
  370.2 45.0 %flash.5 = (bf16[256,1024]{1,0:T(8,128)(2,1)}, bf16[256,1024]{1,0:T(8,128)(2,1)}, bf16[256,1024]{1,0:T(8,128)(2,1)}, bf16[256,1024]{1,0:T(8,128)(2,1)}) custom-call(s32[969]{0:T(1024)} %bitcast.30, bf16[8,1024,256]{2,1,0:T(8,128)(2,1)} %get-tuple-element.72.refs_1_, bf16[2,1024,256]{2,1,0:T(8,128)(2,1)} %get-tuple-element.86.refs_2_, ...), custom_call_target="tpu_custom_call" | custom-call | flops 32212254720 | bytes 8388608 | tf_op jit(solution)/shard_map/flash/pallas_call | solution.py:355
  417.3 11.2 collective-permute-start.18
  430.5 11.1 collective-permute-done.18.refs_2_
  441.6 22.4 %collective-permute-done.27.refs_13_ = bf16[256,4096]{1,0:T(8,128)(2,1)} collective-permute-done((bf16[256,4096]{1,0:T(8,128)(2,1)}, bf16[256,4096]{1,0:T(8,128)(2,1)}, u32[]{:S(2)}, u32[]{:S(2)}) %collective-permute-start.27) | collective-permute-done | bytes 2097184 | tf_op jit(solution)/shard_map/ppermute | solution.py:691
  464.1 11.2 collective-permute-start.21
  475.3 32.4 %collective-permute-done.26.refs_12_ = bf16[256,4096]{1,0:T(8,128)(2,1)} collective-permute-done((bf16[256,4096]{1,0:T(8,128)(2,1)}, bf16[256,4096]{1,0:T(8,128)(2,1)}, u32[]{:S(2)}, u32[]{:S(2)}) %collective-permute-start.26) | collective-permute-done | bytes 2097184 | tf_op jit(solution)/shard_map/ppermute | solution.py:691
  507.7 10.9 collective-permute-start.22
  518.6 44.2 %flash.6 = (bf16[256,1024]{1,0:T(8,128)(2,1)}, bf16[256,1024]{1,0:T(8,128)(2,1)}, bf16[256,1024]{1,0:T(8,128)(2,1)}, bf16[256,1024]{1,0:T(8,128)(2,1)}) custom-call(s32[969]{0:T(1024)} %bitcast.31, bf16[8,1024,256]{2,1,0:T(8,128)(2,1)} %get-tuple-element.72.refs_1_, bf16[2,1024,256]{2,1,0:T(8,128)(2,1)} %get-tuple-element.95.refs_2_, ...), custom_call_target="tpu_custom_call" | custom-call | flops 32212254720 | bytes 8388608 | tf_op jit(solution)/shard_map/flash/pallas_call | solution.py:355
  577.0 29.0 %outp.2 = (bf16[256,4096]{1,0:T(8,128)(2,1)}, bf16[256,4096]{1,0:T(8,128)(2,1)}, bf16[256,4096]{1,0:T(8,128)(2,1)}, bf16[256,4096]{1,0:T(8,128)(2,1)}) custom-call(bf16[256,1024]{1,0:T(8,128)(2,1)} %get-tuple-element.82.refs_14_.refs_0_, bf16[256,1024]{1,0:T(8,128)(2,1)} %collective-permute-done.17.refs_1_, ...), custom_call_target="tpu_custom_call" | custom-call | flops 17179869184 | bytes 33554432 | tf_op jit(solution)/shard_map/outp/pallas_call | solution.py:465
  606.4 43.7 %flash.7 = (bf16[256,1024]{1,0:T(8,128)(2,1)}, bf16[256,1024]{1,0:T(8,128)(2,1)}, bf16[256,1024]{1,0:T(8,128)(2,1)}, bf16[256,1024]{1,0:T(8,128)(2,1)}) custom-call(s32[969]{0:T(1024)} %bitcast.32, bf16[8,1024,256]{2,1,0:T(8,128)(2,1)} %get-tuple-element.72.refs_1_, bf16[2,1024,256]{2,1,0:T(8,128)(2,1)} %qkv.11.refs_14_.refs_2_, ...), custom_call_target="tpu_custom_call" | custom-call | flops 32212254720 | bytes 8388608 | tf_op jit(solution)/shard_map/flash/pallas_call | solution.py:355
  658.9 86.7 %mlp.5 = (bf16[512,4096]{1,0:T(8,128)(2,1)}, bf16[512,4096]{1,0:T(8,128)(2,1)}) custom-call(bf16[256,4096]{1,0:T(8,128)(2,1)} %get-tuple-element.98.refs_0_, bf16[256,4096]{1,0:T(8,128)(2,1)} %collective-permute-done.32.refs_1_, bf16[256,4096]{1,0:T(8,128)(2,1)} %collective-permute-done.33.refs_2_, bf16[256,4096]{1,0:T(8,128)(2,1)} %collective-permute-done.34.refs_3_, ...), custom_call_target="tpu_custom_call" | custom-call | flops 77309411328 | bytes 75497472 | tf_op jit(solution)/shard_map/mlp/pallas_call | solution.py:550
  747.7 6.2 collective-permute-done.36.refs_1_
  754.0 7.2 collective-permute-done.37.refs_2_
  761.6 9.3 collective-permute-done.38.refs_3_
  772.3 11.4 collective-permute-done.40.refs_6_
  783.7 9.6 collective-permute-done.41.refs_7_
  793.3 29.0 %outp.3 = (bf16[256,4096]{1,0:T(8,128)(2,1)}, bf16[256,4096]{1,0:T(8,128)(2,1)}, bf16[256,4096]{1,0:T(8,128)(2,1)}, bf16[256,4096]{1,0:T(8,128)(2,1)}) custom-call(bf16[256,1024]{1,0:T(8,128)(2,1)} %get-tuple-element.96.refs_20_.refs_0_, bf16[256,1024]{1,0:T(8,128)(2,1)} %collective-permute-done.36.refs_1_, ...), custom_call_target="tpu_custom_call" | custom-call | flops 17179869184 | bytes 33554432 | tf_op jit(solution)/shard_map/outp/pallas_call | solution.py:465
  826.7 87.0 %mlp.6 = (bf16[512,4096]{1,0:T(8,128)(2,1)}, bf16[512,4096]{1,0:T(8,128)(2,1)}) custom-call(bf16[256,4096]{1,0:T(8,128)(2,1)} %get-tuple-element.112.refs_0_, bf16[256,4096]{1,0:T(8,128)(2,1)} %collective-permute-done.43.refs_1_, bf16[256,4096]{1,0:T(8,128)(2,1)} %collective-permute-done.44.refs_2_, bf16[256,4096]{1,0:T(8,128)(2,1)} %collective-permute-done.45.refs_3_, ...), custom_call_target="tpu_custom_call" | custom-call | flops 77309411328 | bytes 75497472 | tf_op jit(solution)/shard_map/mlp/pallas_call | solution.py:550
  916.4 46.8 %collective-permute-done.48.refs_1_ = bf16[256,4096]{1,0:T(8,128)(2,1)} collective-permute-done((bf16[256,4096]{1,0:T(8,128)(2,1)}, bf16[256,4096]{1,0:T(8,128)(2,1)}, u32[]{:S(2)}, u32[]{:S(2)}) %collective-permute-start.48) | collective-permute-done | bytes 2097184 | tf_op jit(solution)/shard_map/ppermute | solution.py:691
  963.2 44.0 %collective-permute-done.42.refs_2_ = bf16[256,4096]{1,0:T(8,128)(2,1)} collective-permute-done((bf16[256,4096]{1,0:T(8,128)(2,1)}, bf16[256,4096]{1,0:T(8,128)(2,1)}, u32[]{:S(2)}, u32[]{:S(2)}) %collective-permute-start.42) | collective-permute-done | bytes 2097184 | tf_op jit(solution)/shard_map/ppermute | solution.py:691
  1007.2 5.6 zsum.5.refs_0_
  1017.2 86.8 %mlp.7 = (bf16[512,4096]{1,0:T(8,128)(2,1)}, bf16[512,4096]{1,0:T(8,128)(2,1)}) custom-call(bf16[256,4096]{1,0:T(8,128)(2,1)} %get-tuple-element.118.refs_0_, bf16[256,4096]{1,0:T(8,128)(2,1)} %collective-permute-done.48.refs_1_, bf16[256,4096]{1,0:T(8,128)(2,1)} %collective-permute-done.49.refs_2_, bf16[256,4096]{1,0:T(8,128)(2,1)} %collective-permute-done.50.refs_3_, ...), custom_call_target="tpu_custom_call" | custom-call | flops 77309411328 | bytes 75497472 | tf_op jit(solution)/shard_map/mlp/pallas_call | solution.py:550
  1106.1 46.8 %collective-permute-done.53.refs_1_ = bf16[256,4096]{1,0:T(8,128)(2,1)} collective-permute-done((bf16[256,4096]{1,0:T(8,128)(2,1)}, bf16[256,4096]{1,0:T(8,128)(2,1)}, u32[]{:S(2)}, u32[]{:S(2)}) %collective-permute-start.53) | collective-permute-done | bytes 2097184 | tf_op jit(solution)/shard_map/ppermute | solution.py:691
  1152.9 44.4 %collective-permute-done.47.refs_3_ = bf16[256,4096]{1,0:T(8,128)(2,1)} collective-permute-done((bf16[256,4096]{1,0:T(8,128)(2,1)}, bf16[256,4096]{1,0:T(8,128)(2,1)}, u32[]{:S(2)}, u32[]{:S(2)}) %collective-permute-start.47) | collective-permute-done | bytes 2097184 | tf_op jit(solution)/shard_map/ppermute | solution.py:691
  1197.3 5.8 zsum.6.refs_0_
  1207.8 48.0 %mlp.8 = (bf16[256,4096]{1,0:T(8,128)(2,1)}, bf16[256,4096]{1,0:T(8,128)(2,1)}) custom-call(bf16[256,4096]{1,0:T(8,128)(2,1)} %get-tuple-element.123.refs_0_, bf16[256,4096]{1,0:T(8,128)(2,1)} %collective-permute-done.53.refs_1_, bf16[256,4096]{1,0:T(8,128)(2,1)} %collective-permute-done.54.refs_2_, bf16[256,4096]{1,0:T(8,128)(2,1)} %collective-permute-done.55.refs_3_, ...), custom_call_target="tpu_custom_call" | custom-call | flops 38654705664 | bytes 75497472 | tf_op jit(solution)/shard_map/mlp/pallas_call | solution.py:550
  1255.8 5.6 zsum.7.refs_0_
  1264.2 48.0 %mlp.9 = (bf16[256,4096]{1,0:T(8,128)(2,1)}, bf16[256,4096]{1,0:T(8,128)(2,1)}) custom-call(bf16[256,4096]{1,0:T(8,128)(2,1)} %get-tuple-element.123.refs_0_, bf16[256,4096]{1,0:T(8,128)(2,1)} %collective-permute-done.53.refs_1_, bf16[256,4096]{1,0:T(8,128)(2,1)} %collective-permute-done.54.refs_2_, bf16[256,4096]{1,0:T(8,128)(2,1)} %collective-permute-done.55.refs_3_, ...), custom_call_target="tpu_custom_call" | custom-call | flops 38654705664 | bytes 75497472 | tf_op jit(solution)/shard_map/mlp/pallas_call | solution.py:550
  1322.2 16.8 %collective-permute-done.57.refs_3_ = bf16[128,4096]{1,0:T(8,128)(2,1)} collective-permute-done((bf16[128,4096]{1,0:T(8,128)(2,1)}, bf16[128,4096]{1,0:T(8,128)(2,1)}, u32[]{:S(2)}, u32[]{:S(2)}) %collective-permute-start.57) | collective-permute-done | bytes 1048608 | tf_op jit(solution)/shard_map/ppermute | solution.py:691
  1342.3 18.3 %collective-permute-done.59.refs_3_ = bf16[128,4096]{1,0:T(8,128)(2,1)} collective-permute-done((bf16[128,4096]{1,0:T(8,128)(2,1)}, bf16[128,4096]{1,0:T(8,128)(2,1)}, u32[]{:S(2)}, u32[]{:S(2)}) %collective-permute-start.59) | collective-permute-done | bytes 1048608 | tf_op jit(solution)/shard_map/ppermute | solution.py:691
  (121 shorter events, 115.2 us)
Async XLA Ops:
  4.7 73.0 %collective-permute-start.4 = (bf16[256,4096]{1,0:T(8,128)(2,1)}, bf16[256,4096]{1,0:T(8,128)(2,1)}, u32[]{:S(2)}, u32[]{:S(2)}) collective-permute-start(bf16[256,4096]{1,0:T(8,128)(2,1)} %norm.4.refs_2_.refs_0_), channel_id=1, source_target_pairs={{0,2},{1,3},{2,0},{3,1},{4,6},{5,7},{6,4},{7,5}} | collective-permute-start | bytes 6291464 | tf_op jit(solution)/shard_map/ppermute | solution.py:691
  8.0 30.0 %collective-permute-start = (bf16[256,4096]{1,0:T(8,128)(2,1)}, bf16[256,4096]{1,0:T(8,128)(2,1)}, u32[]{:S(2)}, u32[]{:S(2)}) collective-permute-start(bf16[256,4096]{1,0:T(8,128)(2,1)} %norm.4.refs_2_.refs_0_), channel_id=1, source_target_pairs={{0,1},{1,0},{2,3},{3,2},{4,5},{5,4},{6,7},{7,6}} | collective-permute-start | bytes 6291464 | tf_op jit(solution)/shard_map/ppermute | solution.py:691
  11.5 26.6 %collective-permute-start.1 = (bf16[256,4096]{1,0:T(8,128)(2,1)}, bf16[256,4096]{1,0:T(8,128)(2,1)}, u32[]{:S(2)}, u32[]{:S(2)}) collective-permute-start(bf16[256,4096]{1,0:T(8,128)(2,1)} %norm.5.refs_2_.refs_1_), channel_id=1, source_target_pairs={{0,1},{1,0},{2,3},{3,2},{4,5},{5,4},{6,7},{7,6}} | collective-permute-start | bytes 6291464 | tf_op jit(solution)/shard_map/ppermute | solution.py:691
  15.4 22.6 %collective-permute-start.2 = (bf16[256,4096]{1,0:T(8,128)(2,1)}, bf16[256,4096]{1,0:T(8,128)(2,1)}, u32[]{:S(2)}, u32[]{:S(2)}) collective-permute-start(bf16[256,4096]{1,0:T(8,128)(2,1)} %norm.6.refs_2_), channel_id=1, source_target_pairs={{0,1},{1,0},{2,3},{3,2},{4,5},{5,4},{6,7},{7,6}} | collective-permute-start | bytes 6291464 | tf_op jit(solution)/shard_map/ppermute | solution.py:691
  18.8 19.2 %collective-permute-start.3 = (bf16[256,4096]{1,0:T(8,128)(2,1)}, bf16[256,4096]{1,0:T(8,128)(2,1)}, u32[]{:S(2)}, u32[]{:S(2)}) collective-permute-start(bf16[256,4096]{1,0:T(8,128)(2,1)} %norm.7.refs_3_), channel_id=1, source_target_pairs={{0,1},{1,0},{2,3},{3,2},{4,5},{5,4},{6,7},{7,6}} | collective-permute-start | bytes 6291464 | tf_op jit(solution)/shard_map/ppermute | solution.py:691
  77.8 48.3 %collective-permute-start.6 = (bf16[256,4096]{1,0:T(8,128)(2,1)}, bf16[256,4096]{1,0:T(8,128)(2,1)}, u32[]{:S(2)}, u32[]{:S(2)}) collective-permute-start(bf16[256,4096]{1,0:T(8,128)(2,1)} %norm.5.refs_2_.refs_1_), channel_id=1, source_target_pairs={{0,2},{1,3},{2,0},{3,1},{4,6},{5,7},{6,4},{7,5}} | collective-permute-start | bytes 6291464 | tf_op jit(solution)/shard_map/ppermute | solution.py:691
  126.1 71.8 %collective-permute-start.8 = (bf16[256,4096]{1,0:T(8,128)(2,1)}, bf16[256,4096]{1,0:T(8,128)(2,1)}, u32[]{:S(2)}, u32[]{:S(2)}) collective-permute-start(bf16[256,4096]{1,0:T(8,128)(2,1)} %norm.6.refs_2_), channel_id=1, source_target_pairs={{0,2},{1,3},{2,0},{3,1},{4,6},{5,7},{6,4},{7,5}} | collective-permute-start | bytes 6291464 | tf_op jit(solution)/shard_map/ppermute | solution.py:691
  199.7 47.9 %collective-permute-start.10 = (bf16[256,4096]{1,0:T(8,128)(2,1)}, bf16[256,4096]{1,0:T(8,128)(2,1)}, u32[]{:S(2)}, u32[]{:S(2)}) collective-permute-start(bf16[256,4096]{1,0:T(8,128)(2,1)} %norm.7.refs_3_), channel_id=1, source_target_pairs={{0,2},{1,3},{2,0},{3,1},{4,6},{5,7},{6,4},{7,5}} | collective-permute-start | bytes 6291464 | tf_op jit(solution)/shard_map/ppermute | solution.py:691
  247.6 48.8 %collective-permute-start.12 = (bf16[8,2,256,256]{3,2,1,0:T(8,128)(2,1)}, bf16[8,2,256,256]{3,2,1,0:T(8,128)(2,1)}, u32[]{:S(2)}, u32[]{:S(2)}) collective-permute-start(bf16[8,2,256,256]{3,2,1,0:T(8,128)(2,1)} %get-tuple-element.73.refs_5_.refs_3_), channel_id=1, source_target_pairs={{0,4},{4,0},{1,5},{5,1},{2,6},{6,2},{3,7},{7,3}} | collective-permute-start | bytes 6291464 | tf_op jit(solution)/shard_map/ppermute | solution.py:691
  250.4 57.2 %collective-permute-start.13 = (bf16[2,2,256,256]{3,2,1,0:T(8,128)(2,1)}, bf16[2,2,256,256]{3,2,1,0:T(8,128)(2,1)}, u32[]{:S(2)}, u32[]{:S(2)}) collective-permute-start(bf16[2,2,256,256]{3,2,1,0:T(8,128)(2,1)} %get-tuple-element.76.refs_5_.refs_4_), channel_id=1, source_target_pairs={{0,4},{4,0},{1,5},{5,1},{2,6},{6,2},{3,7},{7,3}} | collective-permute-start | bytes 1572872 | tf_op jit(solution)/shard_map/ppermute | solution.py:691
  251.0 68.0 %collective-permute-start.14 = (bf16[2,2,256,256]{3,2,1,0:T(8,128)(2,1)}, bf16[2,2,256,256]{3,2,1,0:T(8,128)(2,1)}, u32[]{:S(2)}, u32[]{:S(2)}) collective-permute-start(bf16[2,2,256,256]{3,2,1,0:T(8,128)(2,1)} %get-tuple-element.78.refs_5_), channel_id=1, source_target_pairs={{0,4},{4,0},{1,5},{5,1},{2,6},{6,2},{3,7},{7,3}} | collective-permute-start | bytes 1572872 | tf_op jit(solution)/shard_map/ppermute | solution.py:691
  257.3 72.9 %collective-permute-start.15 = (bf16[2,2,256,256]{3,2,1,0:T(8,128)(2,1)}, bf16[2,2,256,256]{3,2,1,0:T(8,128)(2,1)}, u32[]{:S(2)}, u32[]{:S(2)}) collective-permute-start(bf16[2,2,256,256]{3,2,1,0:T(8,128)(2,1)} %get-tuple-element.80.refs_5_.refs_6_), channel_id=1, source_target_pairs={{0,4},{4,0},{1,5},{5,1},{2,6},{6,2},{3,7},{7,3}} | collective-permute-start | bytes 1572872 | tf_op jit(solution)/shard_map/ppermute | solution.py:691
  265.6 75.3 %collective-permute-start.16 = (bf16[2,2,256,256]{3,2,1,0:T(8,128)(2,1)}, bf16[2,2,256,256]{3,2,1,0:T(8,128)(2,1)}, u32[]{:S(2)}, u32[]{:S(2)}) collective-permute-start(bf16[2,2,256,256]{3,2,1,0:T(8,128)(2,1)} %qkv.10.refs_5_.refs_7_), channel_id=1, source_target_pairs={{0,4},{4,0},{1,5},{5,1},{2,6},{6,2},{3,7},{7,3}} | collective-permute-start | bytes 1572872 | tf_op jit(solution)/shard_map/ppermute | solution.py:691
  296.4 274.6 %collective-permute-start.23 = (bf16[1024,4096]{1,0:T(8,128)(2,1)}, bf16[1024,4096]{1,0:T(8,128)(2,1)}, u32[]{:S(2)}, u32[]{:S(2)}) collective-permute-start(bf16[1024,4096]{1,0:T(8,128)(2,1)} %bitcast.23), channel_id=1, source_target_pairs={{0,1},{1,0},{2,3},{3,2},{4,5},{5,4},{6,7},{7,6}} | collective-permute-start | bytes 25165832 | tf_op jit(solution)/shard_map/ppermute | solution.py:691
  307.7 107.6 %collective-permute-start.25 = (bf16[256,4096]{1,0:T(8,128)(2,1)}, bf16[256,4096]{1,0:T(8,128)(2,1)}, u32[]{:S(2)}, u32[]{:S(2)}) collective-permute-start(bf16[256,4096]{1,0:T(8,128)(2,1)} %get-tuple-element.131), channel_id=1, source_target_pairs={{0,2},{1,3},{2,0},{3,1},{4,6},{5,7},{6,4},{7,5}} | collective-permute-start | bytes 6291464 | tf_op jit(solution)/shard_map/ppermute | solution.py:691
  318.9 96.4 %collective-permute-start.24 = (bf16[256,4096]{1,0:T(8,128)(2,1)}, bf16[256,4096]{1,0:T(8,128)(2,1)}, u32[]{:S(2)}, u32[]{:S(2)}) collective-permute-start(bf16[256,4096]{1,0:T(8,128)(2,1)} %get-tuple-element.132), channel_id=1, source_target_pairs={{0,2},{1,3},{2,0},{3,1},{4,6},{5,7},{6,4},{7,5}} | collective-permute-start | bytes 6291464 | tf_op jit(solution)/shard_map/ppermute | solution.py:691
  415.2 48.8 %collective-permute-start.27 = (bf16[256,4096]{1,0:T(8,128)(2,1)}, bf16[256,4096]{1,0:T(8,128)(2,1)}, u32[]{:S(2)}, u32[]{:S(2)}) collective-permute-start(bf16[256,4096]{1,0:T(8,128)(2,1)} %collective-permute-done.25.refs_11_), channel_id=1, source_target_pairs={{0,4},{4,0},{1,5},{5,1},{2,6},{6,2},{3,7},{7,3}} | collective-permute-start | bytes 6291464 | tf_op jit(solution)/shard_map/ppermute | solution.py:691
  415.3 92.4 %collective-permute-start.26 = (bf16[256,4096]{1,0:T(8,128)(2,1)}, bf16[256,4096]{1,0:T(8,128)(2,1)}, u32[]{:S(2)}, u32[]{:S(2)}) collective-permute-start(bf16[256,4096]{1,0:T(8,128)(2,1)} %collective-permute-done.24.refs_10_), channel_id=1, source_target_pairs={{0,4},{4,0},{1,5},{5,1},{2,6},{6,2},{3,7},{7,3}} | collective-permute-start | bytes 6291464 | tf_op jit(solution)/shard_map/ppermute | solution.py:691
  417.3 24.3 %collective-permute-start.18 = (bf16[256,1024]{1,0:T(8,128)(2,1)}, bf16[256,1024]{1,0:T(8,128)(2,1)}, u32[]{:S(2)}, u32[]{:S(2)}) collective-permute-start(bf16[256,1024]{1,0:T(8,128)(2,1)} %get-tuple-element.84), channel_id=1, source_target_pairs={{0,2},{1,3},{2,0},{3,1},{4,6},{5,7},{6,4},{7,5}} | collective-permute-start | bytes 1572872 | tf_op jit(solution)/shard_map/ppermute | solution.py:691
  428.5 134.3 %collective-permute-start.19 = (bf16[256,1024]{1,0:T(8,128)(2,1)}, bf16[256,1024]{1,0:T(8,128)(2,1)}, u32[]{:S(2)}, u32[]{:S(2)}) collective-permute-start(bf16[256,1024]{1,0:T(8,128)(2,1)} %get-tuple-element.85), channel_id=1, source_target_pairs={{0,3},{1,2},{2,1},{3,0},{4,7},{5,6},{6,5},{7,4}} | collective-permute-start | bytes 1572872 | tf_op jit(solution)/shard_map/ppermute | solution.py:691
  441.6 122.3 %collective-permute-start.20 = (bf16[256,1024]{1,0:T(8,128)(2,1)}, bf16[256,1024]{1,0:T(8,128)(2,1)}, u32[]{:S(2)}, u32[]{:S(2)}) collective-permute-start(bf16[256,1024]{1,0:T(8,128)(2,1)} %get-tuple-element.88), channel_id=1, source_target_pairs={{0,1},{1,0},{2,3},{3,2},{4,5},{5,4},{6,7},{7,6}} | collective-permute-start | bytes 1572872 | tf_op jit(solution)/shard_map/ppermute | solution.py:691
  464.1 99.9 %collective-permute-start.21 = (bf16[256,1024]{1,0:T(8,128)(2,1)}, bf16[256,1024]{1,0:T(8,128)(2,1)}, u32[]{:S(2)}, u32[]{:S(2)}) collective-permute-start(bf16[256,1024]{1,0:T(8,128)(2,1)} %get-tuple-element.89), channel_id=1, source_target_pairs={{0,2},{1,3},{2,0},{3,1},{4,6},{5,7},{6,4},{7,5}} | collective-permute-start | bytes 1572872 | tf_op jit(solution)/shard_map/ppermute | solution.py:691
  507.7 56.7 %collective-permute-start.22 = (bf16[256,1024]{1,0:T(8,128)(2,1)}, bf16[256,1024]{1,0:T(8,128)(2,1)}, u32[]{:S(2)}, u32[]{:S(2)}) collective-permute-start(bf16[256,1024]{1,0:T(8,128)(2,1)} %get-tuple-element.90), channel_id=1, source_target_pairs={{0,3},{1,2},{2,1},{3,0},{4,7},{5,6},{6,5},{7,4}} | collective-permute-start | bytes 1572872 | tf_op jit(solution)/shard_map/ppermute | solution.py:691
  564.4 12.6 collective-permute-start.30
  606.0 48.7 %collective-permute-start.33 = (bf16[256,4096]{1,0:T(8,128)(2,1)}, bf16[256,4096]{1,0:T(8,128)(2,1)}, u32[]{:S(2)}, u32[]{:S(2)}) collective-permute-start(bf16[256,4096]{1,0:T(8,128)(2,1)} %get-tuple-element.98.refs_0_), channel_id=1, source_target_pairs={{0,1},{1,0},{2,3},{3,2},{4,5},{5,4},{6,7},{7,6}} | collective-permute-start | bytes 6291464 | tf_op jit(solution)/shard_map/ppermute | solution.py:691
  606.4 48.0 %collective-permute-start.32 = (bf16[256,4096]{1,0:T(8,128)(2,1)}, bf16[256,4096]{1,0:T(8,128)(2,1)}, u32[]{:S(2)}, u32[]{:S(2)}) collective-permute-start(bf16[256,4096]{1,0:T(8,128)(2,1)} %get-tuple-element.98.refs_0_), channel_id=1, source_target_pairs={{0,2},{1,3},{2,0},{3,1},{4,6},{5,7},{6,4},{7,5}} | collective-permute-start | bytes 6291464 | tf_op jit(solution)/shard_map/ppermute | solution.py:691
  654.4 107.1 %collective-permute-start.43 = (bf16[256,4096]{1,0:T(8,128)(2,1)}, bf16[256,4096]{1,0:T(8,128)(2,1)}, u32[]{:S(2)}, u32[]{:S(2)}) collective-permute-start(bf16[256,4096]{1,0:T(8,128)(2,1)} %get-tuple-element.112.refs_0_), channel_id=1, source_target_pairs={{0,2},{1,3},{2,0},{3,1},{4,6},{5,7},{6,4},{7,5}} | collective-permute-start | bytes 6291464 | tf_op jit(solution)/shard_map/ppermute | solution.py:691
  745.6 76.8 %collective-permute-start.35 = (bf16[512,4096]{1,0:T(8,128)(2,1)}, bf16[512,4096]{1,0:T(8,128)(2,1)}, u32[]{:S(2)}, u32[]{:S(2)}) collective-permute-start(bf16[512,4096]{1,0:T(8,128)(2,1)} %get-tuple-element.103), channel_id=1, source_target_pairs={{0,1},{1,0},{2,3},{3,2},{4,5},{5,4},{6,7},{7,6}} | collective-permute-start | bytes 12582920 | tf_op jit(solution)/shard_map/ppermute | solution.py:691
  746.2 15.1 %collective-permute-start.37 = (bf16[256,1024]{1,0:T(8,128)(2,1)}, bf16[256,1024]{1,0:T(8,128)(2,1)}, u32[]{:S(2)}, u32[]{:S(2)}) collective-permute-start(bf16[256,1024]{1,0:T(8,128)(2,1)} %get-tuple-element.105), channel_id=1, source_target_pairs={{0,2},{1,3},{2,0},{3,1},{4,6},{5,7},{6,4},{7,5}} | collective-permute-start | bytes 1572872 | tf_op jit(solution)/shard_map/ppermute | solution.py:691
  746.5 24.4 %collective-permute-start.38 = (bf16[256,1024]{1,0:T(8,128)(2,1)}, bf16[256,1024]{1,0:T(8,128)(2,1)}, u32[]{:S(2)}, u32[]{:S(2)}) collective-permute-start(bf16[256,1024]{1,0:T(8,128)(2,1)} %get-tuple-element.106), channel_id=1, source_target_pairs={{0,3},{1,2},{2,1},{3,0},{4,7},{5,6},{6,5},{7,4}} | collective-permute-start | bytes 1572872 | tf_op jit(solution)/shard_map/ppermute | solution.py:691
  753.9 18.4 %collective-permute-start.39 = (bf16[256,1024]{1,0:T(8,128)(2,1)}, bf16[256,1024]{1,0:T(8,128)(2,1)}, u32[]{:S(2)}, u32[]{:S(2)}) collective-permute-start(bf16[256,1024]{1,0:T(8,128)(2,1)} %get-tuple-element.107), channel_id=1, source_target_pairs={{0,1},{1,0},{2,3},{3,2},{4,5},{5,4},{6,7},{7,6}} | collective-permute-start | bytes 1572872 | tf_op jit(solution)/shard_map/ppermute | solution.py:691
  761.3 22.5 %collective-permute-start.40 = (bf16[256,1024]{1,0:T(8,128)(2,1)}, bf16[256,1024]{1,0:T(8,128)(2,1)}, u32[]{:S(2)}, u32[]{:S(2)}) collective-permute-start(bf16[256,1024]{1,0:T(8,128)(2,1)} %get-tuple-element.108), channel_id=1, source_target_pairs={{0,2},{1,3},{2,0},{3,1},{4,6},{5,7},{6,4},{7,5}} | collective-permute-start | bytes 1572872 | tf_op jit(solution)/shard_map/ppermute | solution.py:691
  761.6 31.8 %collective-permute-start.41 = (bf16[256,1024]{1,0:T(8,128)(2,1)}, bf16[256,1024]{1,0:T(8,128)(2,1)}, u32[]{:S(2)}, u32[]{:S(2)}) collective-permute-start(bf16[256,1024]{1,0:T(8,128)(2,1)} %get-tuple-element.109), channel_id=1, source_target_pairs={{0,3},{1,2},{2,1},{3,0},{4,7},{5,6},{6,5},{7,4}} | collective-permute-start | bytes 1572872 | tf_op jit(solution)/shard_map/ppermute | solution.py:691
  770.9 55.8 %collective-permute-start.44 = (bf16[256,4096]{1,0:T(8,128)(2,1)}, bf16[256,4096]{1,0:T(8,128)(2,1)}, u32[]{:S(2)}, u32[]{:S(2)}) collective-permute-start(bf16[256,4096]{1,0:T(8,128)(2,1)} %get-tuple-element.112.refs_0_), channel_id=1, source_target_pairs={{0,1},{1,0},{2,3},{3,2},{4,5},{5,4},{6,7},{7,6}} | collective-permute-start | bytes 6291464 | tf_op jit(solution)/shard_map/ppermute | solution.py:691
  772.3 54.4 %collective-permute-start.45 = (bf16[256,4096]{1,0:T(8,128)(2,1)}, bf16[256,4096]{1,0:T(8,128)(2,1)}, u32[]{:S(2)}, u32[]{:S(2)}) collective-permute-start(bf16[256,4096]{1,0:T(8,128)(2,1)} %collective-permute-done.43.refs_1_), channel_id=1, source_target_pairs={{0,1},{1,0},{2,3},{3,2},{4,5},{5,4},{6,7},{7,6}} | collective-permute-start | bytes 6291464 | tf_op jit(solution)/shard_map/ppermute | solution.py:691
  913.7 99.1 %collective-permute-start.46 = (bf16[512,4096]{1,0:T(8,128)(2,1)}, bf16[512,4096]{1,0:T(8,128)(2,1)}, u32[]{:S(2)}, u32[]{:S(2)}) collective-permute-start(bf16[512,4096]{1,0:T(8,128)(2,1)} %get-tuple-element.115), channel_id=1, source_target_pairs={{0,1},{1,0},{2,3},{3,2},{4,5},{5,4},{6,7},{7,6}} | collective-permute-start | bytes 12582920 | tf_op jit(solution)/shard_map/ppermute | solution.py:691
  914.4 48.8 %collective-permute-start.48 = (bf16[256,4096]{1,0:T(8,128)(2,1)}, bf16[256,4096]{1,0:T(8,128)(2,1)}, u32[]{:S(2)}, u32[]{:S(2)}) collective-permute-start(bf16[256,4096]{1,0:T(8,128)(2,1)} %get-tuple-element.118.refs_0_), channel_id=1, source_target_pairs={{0,2},{1,3},{2,0},{3,1},{4,6},{5,7},{6,4},{7,5}} | collective-permute-start | bytes 6291464 | tf_op jit(solution)/shard_map/ppermute | solution.py:691
  914.7 92.5 %collective-permute-start.42 = (bf16[256,4096]{1,0:T(8,128)(2,1)}, bf16[256,4096]{1,0:T(8,128)(2,1)}, u32[]{:S(2)}, u32[]{:S(2)}) collective-permute-start(bf16[256,4096]{1,0:T(8,128)(2,1)} %add_convert_fusion.2.refs_7_), channel_id=1, source_target_pairs={{0,2},{1,3},{2,0},{3,1},{4,6},{5,7},{6,4},{7,5}} | collective-permute-start | bytes 6291464 | tf_op jit(solution)/shard_map/ppermute | solution.py:691
  916.4 100.8 %collective-permute-start.49 = (bf16[256,4096]{1,0:T(8,128)(2,1)}, bf16[256,4096]{1,0:T(8,128)(2,1)}, u32[]{:S(2)}, u32[]{:S(2)}) collective-permute-start(bf16[256,4096]{1,0:T(8,128)(2,1)} %get-tuple-element.118.refs_0_), channel_id=1, source_target_pairs={{0,1},{1,0},{2,3},{3,2},{4,5},{5,4},{6,7},{7,6}} | collective-permute-start | bytes 6291464 | tf_op jit(solution)/shard_map/ppermute | solution.py:691
  963.2 54.0 %collective-permute-start.50 = (bf16[256,4096]{1,0:T(8,128)(2,1)}, bf16[256,4096]{1,0:T(8,128)(2,1)}, u32[]{:S(2)}, u32[]{:S(2)}) collective-permute-start(bf16[256,4096]{1,0:T(8,128)(2,1)} %collective-permute-done.48.refs_1_), channel_id=1, source_target_pairs={{0,1},{1,0},{2,3},{3,2},{4,5},{5,4},{6,7},{7,6}} | collective-permute-start | bytes 6291464 | tf_op jit(solution)/shard_map/ppermute | solution.py:691
  1104.0 99.1 %collective-permute-start.51 = (bf16[512,4096]{1,0:T(8,128)(2,1)}, bf16[512,4096]{1,0:T(8,128)(2,1)}, u32[]{:S(2)}, u32[]{:S(2)}) collective-permute-start(bf16[512,4096]{1,0:T(8,128)(2,1)} %get-tuple-element.121), channel_id=1, source_target_pairs={{0,1},{1,0},{2,3},{3,2},{4,5},{5,4},{6,7},{7,6}} | collective-permute-start | bytes 12582920 | tf_op jit(solution)/shard_map/ppermute | solution.py:691
  1104.0 48.8 %collective-permute-start.53 = (bf16[256,4096]{1,0:T(8,128)(2,1)}, bf16[256,4096]{1,0:T(8,128)(2,1)}, u32[]{:S(2)}, u32[]{:S(2)}) collective-permute-start(bf16[256,4096]{1,0:T(8,128)(2,1)} %get-tuple-element.123.refs_0_), channel_id=1, source_target_pairs={{0,2},{1,3},{2,0},{3,1},{4,6},{5,7},{6,4},{7,5}} | collective-permute-start | bytes 6291464 | tf_op jit(solution)/shard_map/ppermute | solution.py:691
  1104.3 93.0 %collective-permute-start.47 = (bf16[256,4096]{1,0:T(8,128)(2,1)}, bf16[256,4096]{1,0:T(8,128)(2,1)}, u32[]{:S(2)}, u32[]{:S(2)}) collective-permute-start(bf16[256,4096]{1,0:T(8,128)(2,1)} %add_convert_fusion.1.refs_7_), channel_id=1, source_target_pairs={{0,2},{1,3},{2,0},{3,1},{4,6},{5,7},{6,4},{7,5}} | collective-permute-start | bytes 6291464 | tf_op jit(solution)/shard_map/ppermute | solution.py:691
  1106.1 101.7 %collective-permute-start.54 = (bf16[256,4096]{1,0:T(8,128)(2,1)}, bf16[256,4096]{1,0:T(8,128)(2,1)}, u32[]{:S(2)}, u32[]{:S(2)}) collective-permute-start(bf16[256,4096]{1,0:T(8,128)(2,1)} %get-tuple-element.123.refs_0_), channel_id=1, source_target_pairs={{0,1},{1,0},{2,3},{3,2},{4,5},{5,4},{6,7},{7,6}} | collective-permute-start | bytes 6291464 | tf_op jit(solution)/shard_map/ppermute | solution.py:691
  1152.9 54.9 %collective-permute-start.55 = (bf16[256,4096]{1,0:T(8,128)(2,1)}, bf16[256,4096]{1,0:T(8,128)(2,1)}, u32[]{:S(2)}, u32[]{:S(2)}) collective-permute-start(bf16[256,4096]{1,0:T(8,128)(2,1)} %collective-permute-done.53.refs_1_), channel_id=1, source_target_pairs={{0,1},{1,0},{2,3},{3,2},{4,5},{5,4},{6,7},{7,6}} | collective-permute-start | bytes 6291464 | tf_op jit(solution)/shard_map/ppermute | solution.py:691
  1207.5 48.3 %collective-permute-start.52 = (bf16[256,4096]{1,0:T(8,128)(2,1)}, bf16[256,4096]{1,0:T(8,128)(2,1)}, u32[]{:S(2)}, u32[]{:S(2)}) collective-permute-start(bf16[256,4096]{1,0:T(8,128)(2,1)} %add_convert_fusion.refs_7_), channel_id=1, source_target_pairs={{0,2},{1,3},{2,0},{3,1},{4,6},{5,7},{6,4},{7,5}} | collective-permute-start | bytes 6291464 | tf_op jit(solution)/shard_map/ppermute | solution.py:691
  1312.7 26.3 %collective-permute-start.57 = (bf16[128,4096]{1,0:T(8,128)(2,1)}, bf16[128,4096]{1,0:T(8,128)(2,1)}, u32[]{:S(2)}, u32[]{:S(2)}) collective-permute-start(bf16[128,4096]{1,0:T(8,128)(2,1)} %add_convert_fusion.4.refs_7_), channel_id=1, source_target_pairs={{0,2},{1,3},{2,0},{3,1},{4,6},{5,7},{6,4},{7,5}} | collective-permute-start | bytes 3145736 | tf_op jit(solution)/shard_map/ppermute | solution.py:691
  1320.4 40.1 %collective-permute-start.59 = (bf16[128,4096]{1,0:T(8,128)(2,1)}, bf16[128,4096]{1,0:T(8,128)(2,1)}, u32[]{:S(2)}, u32[]{:S(2)}) collective-permute-start(bf16[128,4096]{1,0:T(8,128)(2,1)} %add_convert_fusion.3.refs_5_), channel_id=1, source_target_pairs={{0,2},{1,3},{2,0},{3,1},{4,6},{5,7},{6,4},{7,5}} | collective-permute-start | bytes 3145736 | tf_op jit(solution)/shard_map/ppermute | solution.py:691
  (15 other events, 89.6 us)

commit v9 on v8

--- a/solution.py
+++ b/solution.py
@@ -13,7 +13,6 @@
 HD = 128
 RUN = 256
 NEG = -1e30
-FAR = 1 << 29
 LOG2E = math.log2(math.e)
 DN = (((1,), (0,)), ((), ()))
 VMEM = 67043328
@@ -138,22 +137,25 @@
     )(*rows, w_all, cos, sin, *after)
 
 
-BLK = 12
+BLK = 11
 LAST, FIRST, CARRY = 16, 32, 64
 ST = HD + 16
 
 
-def flash_kernel(tab_ref, *refs, q_src, kv_src, n_q, n_kv, st_src, n_st, base, G, n_tiles, n_heads, final):
+def flash_kernel(tab_ref, *refs, q_src, kv_src, n_q, n_kv, st_src, n_st, n_old, n_cut, slot, base, G, n_tiles, n_heads, final):
     qs, kvs, sts = refs[:n_q], refs[n_q:n_q + n_kv], refs[n_q + n_kv:n_q + n_kv + n_st]
-    n_out = n_tiles if final else 1
-    at = n_q + n_kv + n_st
+    n_out = n_tiles + 1 if final else 1 + n_cut
+    at = n_q + n_kv + n_st + n_old
     outs = refs[at:at + n_out]
-    q_scr, kv_scr, o_scr, st_scr, s_scr, mb_scr, acc_scr, m_scr, l_scr, q_sem, kv_sem, o_sem, st_sem = refs[at + n_out:]
+    q_scr, kv_scr, o_scr, st_scr, s_scr, mb_scr, acc_scr, m_scr, l_scr, q_sem, kv_sem, o_sem, st_sem = refs[at + n_out:][:13]
+    if n_cut:
+        cut_ref, (cut_scr, cut_sem) = refs[at - 1], refs[-2:]
     T = RUN
     c = (HD ** -0.5) * LOG2E
     n_blocks = tab_ref[base]
-    carried = base + 1 + n_tiles
-    row0 = base + 1 + 2 * n_tiles
+    carried = base + 1
+    row0 = carried + n_tiles
+    null = len(kv_src)
 
     q_copies = [pltpu.make_async_copy(qs[a].at[i], q_scr.at[t], q_sem.at[t]) for t, (a, i) in enumerate(q_src)]
     kv_copies = [pltpu.make_async_copy(kvs[a].at[i], kv_scr.at[r], kv_sem.at[r]) for r, (a, i) in enumerate(kv_src)]
@@ -170,6 +172,13 @@
                 pltpu.make_async_copy(sts[0].at[i], st_scr.at[t], st_sem.at[t]).start()
     for cp in kv_copies[first:]:
         cp.start()
+    kv_scr[null, 1] = jnp.zeros((256, 256), BF)
+    if n_cut:
+        cut_in = pltpu.make_async_copy(cut_ref.at[pl.ds(lax.axis_index('cp') * cut_scr.shape[0], cut_scr.shape[0]), :], cut_scr,
+                                       cut_sem)
+        part = cut_scr.shape[0] // n_cut
+        cut_out = [pltpu.make_async_copy(cut_scr.at[pl.ds(k * part, part), :], outs[1 + k], cut_sem) for k in range(n_cut)]
+        cut_in.start()
 
     def block(i):
         g = lax.div(i, n_blocks)
@@ -205,25 +214,24 @@
         alpha = jnp.exp2(m_prev * c - m_c)
         l, pv = l_scr[h] * alpha, None
         for k in range(4):
+            run = tab_ref[row + 7 + k]
             p = jnp.exp2(s_scr[h, k * RUN:(k + 1) * RUN].reshape(RUN // 8, 8, T) * c - m_c[None])
-            l = l + jnp.sum(p, axis=0)
-            d = lax.dot_general(kv_scr[tab_ref[row + 3 + k], 1, pl.ds(col, HD), :], p.reshape(RUN, T).astype(BF), DN,
+            l = l + jnp.sum(p, axis=0) * jnp.where(run < 0, 0.0, 1.0)
+            d = lax.dot_general(kv_scr[jnp.where(run < 0, null, run), 1, pl.ds(col, HD), :], p.reshape(RUN, T).astype(BF), DN,
                                 preferred_element_type=F32)
             pv = d if pv is None else pv + d
         l_scr[h] = l
         acc_scr[h] = (acc_scr[h].reshape(HD // 8, 8, T) * alpha[None]).reshape(HD, T) + pv
 
-    def mask_runs(row, flags):
-        qry = lax.broadcasted_iota(jnp.int32, (RUN, T), 1) + tab_ref[base + 1 + tab_ref[row]]
-        key = lax.broadcasted_iota(jnp.int32, (RUN, T), 0)
+    def mask_runs(flags):
+        seen = lax.broadcasted_iota(jnp.int32, (RUN, T), 0) <= lax.broadcasted_iota(jnp.int32, (RUN, T), 1)
 
         def one(k, carry):
             @pl.when((lax.shift_right_logical(flags, k) & 1) != 0)
             def _():
-                mask = key + tab_ref[row + 7 + k] <= qry
                 rows = pl.multiple_of(k * RUN, RUN)
                 for h in range(G):
-                    put(jnp.where(mask, s_scr[h, pl.ds(rows, RUN), :], NEG), h, k)
+                    put(jnp.where(seen, s_scr[h, pl.ds(rows, RUN), :], NEG), h, k)
 
             return carry
 
@@ -239,7 +247,7 @@
             for k in range(n_tiles):
                 @pl.when(tile == k)
                 def _():
-                    pltpu.make_async_copy(o_scr.at[k], outs[k], o_sem.at[k]).start()
+                    pltpu.make_async_copy(o_scr.at[k], outs[k].at[slot], o_sem.at[k]).start()
 
     if final and n_st:
         def idle(i, carry):
@@ -297,9 +305,16 @@
                     m_scr[h] = st_scr[tile, g, h, HD:HD + 8, :]
                     l_scr[h] = st_scr[tile, g, h, HD + 8:, :]
 
+        if n_cut:
+            @pl.when(i == n_blocks)
+            def _():
+                cut_in.wait()
+                for cp in cut_out:
+                    cp.start()
+
         @pl.when((flags & 15) != 0)
         def _():
-            mask_runs(row, flags)
+            mask_runs(flags)
 
         for h in range(G):
             stage_b(row, g, h)
@@ -325,7 +340,7 @@
     arrived(have, len(kv_src))
     if final:
         for k in range(n_tiles):
-            pltpu.make_async_copy(o_scr.at[k], outs[k], o_sem.at[k]).wait()
+            pltpu.make_async_copy(o_scr.at[k], outs[k].at[slot], o_sem.at[k]).wait()
     else:
         def wait_out(i, carry):
             row = row0 + BLK * i
@@ -338,30 +353,43 @@
             return carry
 
         lax.fori_loop(0, n_blocks, wait_out, 0)
-
-
-def flash(tab, qs, q_src, kvs, *, base, work, st=None, st_src=None, st_tiles=None, after=()):
+        for cp in cut_out:
+            cp.wait()
+
+
+def flash(tab, qs, q_src, kvs, *, base, work, st=None, st_src=None, old=None, cut=None, n_cut=0, slots=1, after=()):
     nq = qs[0].shape[1]
     n_heads = 2
     G = nq // HD // n_heads
     n_tiles = len(q_src)
-    final = st_tiles is None
+    final = cut is None
     kv_src = [(a, i) for a, kv in enumerate(kvs) for i in range(kv.shape[0])]
     n_runs = len(kv_src)
     sts = () if st is None else (st,)
-    n_in = 1 + len(qs) + len(kvs) + len(sts)
+    old = old or ()
+    more = (*old, *(() if final else (cut,)))
+    n_in = 1 + len(qs) + len(kvs) + len(sts) + len(more)
     state = (n_heads, G, ST, RUN)
     has_st = not final or sts
+    if final:
+        out_shape = [jax.ShapeDtypeStruct((slots, RUN, nq), BF)] * n_tiles + [jax.ShapeDtypeStruct((8, HD), F32)]
+        scratch = []
+    else:
+        half = cut.shape[0] // 2
+        out_shape = [jax.ShapeDtypeStruct((n_tiles, *state), F32)]
+        out_shape += [jax.ShapeDtypeStruct((half // n_cut, cut.shape[1]), BF)] * n_cut
+        scratch = [pltpu.VMEM((half, cut.shape[1]), BF), pltpu.SemaphoreType.DMA]
     return pl.pallas_call(
         ordered(functools.partial(flash_kernel, q_src=q_src, kv_src=kv_src, n_q=len(qs), n_kv=len(kvs),
-                                  st_src=st_src or [None] * n_tiles, n_st=len(sts), base=base, G=G, n_tiles=n_tiles,
-                                  n_heads=n_heads, final=final), n_in, after),
+                                  st_src=st_src or [None] * n_tiles, n_st=len(sts), n_old=len(more), n_cut=n_cut,
+                                  slot=slots - 1 if old else 0, base=base, G=G, n_tiles=n_tiles, n_heads=n_heads, final=final),
+                n_in, after),
         grid_spec=pltpu.PrefetchScalarGridSpec(
             num_scalar_prefetch=1, grid=(),
             in_specs=[ANY] * (n_in - 1 + len(after)),
-            out_specs=[ANY] * n_tiles if final else [ANY],
+            out_specs=[ANY] * len(out_shape),
             scratch_shapes=[pltpu.VMEM((n_tiles, nq, RUN), BF),
-                            pltpu.VMEM((n_runs, 2, 256, 256), BF),
+                            pltpu.VMEM((n_runs + 1, 2, 256, 256), BF),
                             pltpu.VMEM((n_tiles if final else 1, RUN, nq), BF),
                             pltpu.VMEM((n_tiles if has_st else 1, *state), F32),
                             pltpu.VMEM((G, 4 * RUN, RUN), F32),
@@ -372,21 +400,20 @@
                             pltpu.SemaphoreType.DMA((n_tiles,)),
                             pltpu.SemaphoreType.DMA((n_runs,)),
                             pltpu.SemaphoreType.DMA((n_tiles,)),
-                            pltpu.SemaphoreType.DMA((n_tiles,))]),
-        out_shape=[jax.ShapeDtypeStruct((RUN, nq), BF)] * n_tiles if final
-        else [jax.ShapeDtypeStruct((st_tiles, *state), F32)],
-        input_output_aliases={n_in - 1: 0} if sts and not final else {},
+                            pltpu.SemaphoreType.DMA((n_tiles,)), *scratch]),
+        out_shape=out_shape,
+        input_output_aliases={n_in - len(old) + k: k for k in range(len(old))},
         name="flash" if final else "flash_part", compiler_params=params(0),
         cost_estimate=cost(8 * work * RUN * RUN * nq, n_runs * RUN * nq),
-    )(tab, *qs, *kvs, *sts, *after)
+    )(tab, *qs, *kvs, *sts, *more, *after)
 
 
 def out_kernel(*refs, blocks, n_w, n_run, at):
-    n_o, n_out = 4 * n_run, 2 * n_run
+    n_o, n_out = 4, 2 * n_run
     o_refs, w_refs, x_ref, g_ref = refs[:n_o], refs[n_o:n_o + n_w], refs[n_o + n_w], refs[n_o + n_w + 1]
     outs = refs[n_o + n_w + 2:n_o + n_w + 2 + n_out]
     o_scr, w_scr, x_scr, acc_scr, o_sem, w_sem, x_sem, out_sem = refs[n_o + n_w + 2 + n_out:]
-    width = o_refs[0].shape[1]
+    width = o_refs[0].shape[-1]
     half = width // 2
     n_slots = w_scr.shape[0]
 
@@ -405,7 +432,7 @@
     for i in range(n_run):
         rows = pl.ds(i * RUN, RUN)
         for k in range(4):
-            src = o_refs[4 * i + k]
+            src = o_refs[k].at[i]
             if k < 2:
                 loads[2 * k].append((src, o_scr.at[rows, pl.ds(k * width, width)]))
             else:
@@ -459,8 +486,7 @@
 
 def out_proj(os, ws, blocks, x_rows, gain, at, after=()):
     dim = x_rows.shape[1]
-    width = os[0].shape[1]
-    n_run = len(os) // 4
+    n_run, _, width = os[0].shape
     rows = n_run * RUN
     return pl.pallas_call(
         ordered(functools.partial(out_kernel, blocks=blocks, n_w=len(ws), n_run=n_run, at=at),
@@ -593,39 +619,33 @@
     return out
 
 
-def block_list(tile, ids, pos, diag):
-    runs = [(r, pos[r]) for r in ids]
-    if diag is not None:
-        n_tail = (len(runs) % 4) + 1
-        tail = [(diag, pos[diag])] + runs[len(runs) - (n_tail - 1):]
-        runs = runs[:len(runs) - (n_tail - 1)]
-    else:
-        n_tail = len(runs) % 4
-        tail = runs[len(runs) - n_tail:]
-        runs = runs[:len(runs) - n_tail]
-    blocks = [[0, runs[i:i + 4]] for i in range(0, len(runs), 4)]
-    if tail:
-        full = tail + [(tail[0][0], FAR)] * (4 - len(tail))
-        flags = sum(1 << k for k, (r, p) in enumerate(full) if p == FAR or r == diag)
-        blocks.append([flags, full])
+def block_list(tile, ids, diag):
+    own = [] if diag is None else [diag]
+    n_tail = (len(ids) + len(own)) % 4 or 4
+    n_tail -= len(own)
+    head, tail = ids[:len(ids) - n_tail], own + ids[len(ids) - n_tail:]
+    blocks = [[0, head[i:i + 4], head[i:i + 4]] for i in range(0, len(head), 4)]
+    fill = 4 - len(tail)
+    keys = tail + [ids[-1] if ids else diag] * fill
+    blocks.append([sum(1 << k for k, r in enumerate(keys) if r == diag), keys, tail + [-1] * fill])
     blocks[-1][0] |= LAST
     blocks[0][0] |= FIRST
-    return [[tile, flags, 0] + [r for r, _ in four] + [p for _, p in four] + [0] for flags, four in blocks]
-
-
-def call_table(tiles, pos, pairs, carry, idle):
+    return [[tile, flags, 0] + keys + values for flags, keys, values in blocks]
+
+
+def call_table(tiles, pairs, carry, idle):
     rows, most = [], 0
     carry = [c if pairs[t][0] or pairs[t][1] else idle for t, c in enumerate(carry)]
     for t, tile in enumerate(tiles):
         ids, own = pairs[t]
         if ids or own:
-            mine = block_list(t, ids, pos, tile if own else None)
+            mine = block_list(t, ids, tile if own else None)
             mine[0][1] |= CARRY if carry[t] else 0
             rows += mine
     for row in rows:
         most = max(most, max(row[3:7]) + 1)
         row[2] = most
-    return [len(rows)] + [pos[t] for t in tiles] + carry + [v for row in rows for v in row], len(rows)
+    return [len(rows)] + carry + [v for row in rows for v in row], len(rows)
 
 
 def work_tables(cps, piece):
@@ -655,7 +675,7 @@
                                 when[r] = 1
                         pairs.append(([r for r in seen if when[r] == now], stage(t) == now))
                         carry.append(int(stage(t) < now))
-                    tab, n = call_table(tiles, pos, pairs, carry, 2 if now == 1 else 0)
+                    tab, n = call_table(tiles, pairs, carry, 2 if now == 1 else 0)
                     tabs[-1].append(tab)
                     sizes[-1].append(n)
     widths = [max(len(t[k]) for t in tabs) for k in range(len(calls))]
@@ -721,14 +741,12 @@
         half = wo.shape[0] // 2
         n_piece = 2
         rows = half // n_piece
-        wo_gated = tied(wo, kvs[-1])
-        wo_x = [send(over_x, lax.dynamic_slice_in_dim(wo_gated, y_id * half + p * rows, rows, axis=0))
-                for p in range(n_piece)]
-        wo_c = send(over_core, wo_gated)
+        wo_c = send(over_core, tied(wo, kvs[-1]))
 
         tiles = [(0, i) for i in range(2 * n_run)] + [(1, 0), (1, 1)]
-        st, = flash(tab, [q_here, q_far[0]], tiles, kvs[:2], base=bases[0], work=int(work[0]),
-                   st_tiles=len(tiles), after=(kvs[-1],))
+        st, *wo_x = flash(tab, [q_here, q_far[0]], tiles, kvs[:2], base=bases[0], work=int(work[0]), cut=wo,
+                         n_cut=n_piece, after=(kvs[-1],))
+        wo_x = [send(over_x, w) for w in wo_x]
         far_qkv(3, far_qkv(2, st))
         kvs = kvs + [send(over_y, kv) for kv in kvs]
 
@@ -747,11 +765,15 @@
         def attend(j):
             held = 2 * n_run + 2 * j
             carried = [j, n_run + j] + ([held, held + 1] if j == 0 else [None, None])
-            o_own, o_mate, o_far, o_fm = flash(
+            pair = j % 2
+            *o, done = flash(
                 tab, [q_here, q_far[j]], [(0, j), (0, n_run + j), (1, 0), (1, 1)], kvs,
-                base=bases[1 + j], work=int(work[1 + j]), st=st, st_src=carried, after=(prev,))
-            os.append([o_own, send(over_core, o_mate), send(over_x, o_far), send(over_both, o_fm)])
-            return o_own
+                base=bases[1 + j], work=int(work[1 + j]), st=st, st_src=carried, old=os.pop() if pair else None, slots=2,
+                after=(prev,))
+            if pair:
+                o = [o[0], send(over_core, o[1]), send(over_x, o[2]), send(over_both, o[3])]
+            os.append(o)
+            return done
 
         def project(i):
             ws = [wo, wo_c]
@@ -760,7 +782,7 @@
                 for held in (wo_ya, wo_yb):
                     blocks.append([(len(ws) + p, 0, rows) for p in range(n_piece)])
                     ws += [held[p][k] for p in range(n_piece)]
-            got = out_proj(os[2 * i] + os[2 * i + 1], ws, blocks, x_rows, gm, i, after=(prev,))
+            got = out_proj(os[i], ws, blocks, x_rows, gm, i, after=(prev,))
             for y, b in zip(got[::2], got[1::2]):
                 outs.append((y, b, send(over_x, b), send(over_core, b)))
             return got[0]

time: 1370 us -> 1330 us (0.971)
  starting transfers between devices: 65.4 us -> 40.9 us
    ppermute x60 -> x54, starting transfers between devices: 65.4 us -> 40.9 us  [send(): return lax.ppermute(v, *axis_pairs)]
    ppermute x60 -> x54, waiting for transfers between devices: 483 us -> 470 us  [send(): return lax.ppermute(v, *axis_pairs)]
  transfers between devices with their start and end apart: 60 -> 54, of which waited for: 31 -> 27; matrix products, arithmetic and copies ran while one was open for 3% -> 3% of each run, Pallas kernels for 37% -> 32%
where the time goes in v9:
time: 1330 us; the launch traced here: 1320 us
  Pallas kernels  763 us (57%)
  waiting for transfers between devices  470 us (35%)
  starting transfers between devices  40.9 us (3%)
  other arithmetic  23.2 us (2%)
  local copies, waits for them, and re-layouts  19.2 us (1%)
    ppermute x54, waiting for transfers between devices, send(): return lax.ppermute(v, *axis_pairs)  470 us
    pallas_call x5, Pallas kernels, mlp(): pl.pallas_call(ordered(functools.partial(mlp_kernel, n_in=len(bs), first=...  356 us
    pallas_call x5, Pallas kernels, flash(): pl.pallas_call(ordered(functools.partial(flash_kernel, q_src=q_src, kv_sr...  211 us
    pallas_call x6, Pallas kernels, qkv(): pl.pallas_call(ordered(functools.partial(qkv_kernel, n_in=n_in, n_q=n_q,...  101 us
    pallas_call x2, Pallas kernels, out_proj(): pl.pallas_call(ordered(functools.partial(out_kernel, blocks=blocks, n_w=l...  58.1 us
    ppermute x54, starting transfers between devices, send(): return lax.ppermute(v, *axis_pairs)  40.9 us
  transfers between devices with their start and end apart: 54, of which 27 were waited for; matrix products, arithmetic and copies ran while one was open for 3% of the time, Pallas kernels for 32%

profile of v9, /device:TPU:0, one launch (start us, length us, event | category | flops | bytes accessed | tf_op | source)
XLA Modules:
  0.0 1317.9 jit_solution(15337355626959872712)
XLA Ops:
  20.2 9.3 bitcast_dynamic-update-slice_fusion
  29.5 4.8 multiply_sine_fusion
  38.2 39.7 %qkv.6 = (bf16[8,1024,256]{2,1,0:T(8,128)(2,1)}, bf16[8,2,256,256]{3,2,1,0:T(8,128)(2,1)}) custom-call(bf16[256,4096]{1,0:T(8,128)(2,1)} %norm.4.refs_2_.refs_0_, bf16[256,4096]{1,0:T(8,128)(2,1)} %norm.5.refs_2_.refs_1_, bf16[256,4096]{1,0:T(8,128)(2,1)} %norm.6.refs_2_, bf16[256,4096]{1,0:T(8,128)(2,1)} %norm.7.refs_3_, ...), custom_call_target="tpu_custom_call" | custom-call | flops 25769803776 | bytes 12582912 | tf_op jit(solution)/shard_map/qkv/pallas_call | solution.py:126
  78.0 4.5 collective-permute-done.6.refs_1_
  82.5 14.1 %qkv.7 = (bf16[2,1024,256]{2,1,0:T(8,128)(2,1)}, bf16[2,2,256,256]{3,2,1,0:T(8,128)(2,1)}) custom-call(bf16[256,4096]{1,0:T(8,128)(2,1)} %collective-permute-done.5.refs_0_, bf16[256,4096]{1,0:T(8,128)(2,1)} %collective-permute-done.6.refs_1_, bf16[4096,1536]{1,0:T(8,128)(2,1)} %bitcast_dynamic-update-slice_fusion.1.refs_8_.refs_2_, ...), custom_call_target="tpu_custom_call" | custom-call | flops 6442450944 | bytes 12582912 | tf_op jit(solution)/shard_map/qkv/pallas_call | solution.py:126
  96.6 29.7 %collective-permute-done.4.refs_0_ = bf16[256,4096]{1,0:T(8,128)(2,1)} collective-permute-done((bf16[256,4096]{1,0:T(8,128)(2,1)}, bf16[256,4096]{1,0:T(8,128)(2,1)}, u32[]{:S(2)}, u32[]{:S(2)}) %collective-permute-start.4) | collective-permute-done | bytes 2097184 | tf_op jit(solution)/shard_map/ppermute | solution.py:711
  130.8 14.3 %qkv.8 = (bf16[2,1024,256]{2,1,0:T(8,128)(2,1)}, bf16[2,2,256,256]{3,2,1,0:T(8,128)(2,1)}) custom-call(bf16[256,4096]{1,0:T(8,128)(2,1)} %collective-permute-done.4.refs_0_, bf16[256,4096]{1,0:T(8,128)(2,1)} %collective-permute-done.7.refs_1_, bf16[4096,1536]{1,0:T(8,128)(2,1)} %bitcast_dynamic-update-slice_fusion.1.refs_8_.refs_2_, ...), custom_call_target="tpu_custom_call" | custom-call | flops 6442450944 | bytes 12582912 | tf_op jit(solution)/shard_map/qkv/pallas_call | solution.py:126
  145.1 49.9 %flash_part.1 = (f32[10,2,4,144,256]{4,3,2,1,0:T(8,128)}, bf16[256,4096]{1,0:T(8,128)(2,1)}, bf16[256,4096]{1,0:T(8,128)(2,1)}) custom-call(s32[867]{0:T(1024)} %dynamic-slice_reduce_fusion.refs_0_, bf16[8,1024,256]{2,1,0:T(8,128)(2,1)} %get-tuple-element.79.refs_1_, bf16[2,1024,256]{2,1,0:T(8,128)(2,1)} %get-tuple-element.86.refs_2_, ...), custom_call_target="tpu_custom_call" | custom-call | flops 38654705664 | bytes 2621440 | tf_op jit(solution)/shard_map/flash_part/pallas_call | solution.py:382
  196.7 4.1 collective-permute-done.9.refs_1_
  200.8 14.1 %qkv.9 = (bf16[2,1024,256]{2,1,0:T(8,128)(2,1)}, bf16[2,2,256,256]{3,2,1,0:T(8,128)(2,1)}) custom-call(bf16[256,4096]{1,0:T(8,128)(2,1)} %collective-permute-done.8.refs_0_, bf16[256,4096]{1,0:T(8,128)(2,1)} %collective-permute-done.9.refs_1_, bf16[4096,1536]{1,0:T(8,128)(2,1)} %bitcast_dynamic-update-slice_fusion.1.refs_8_.refs_2_, ...), custom_call_target="tpu_custom_call" | custom-call | flops 6442450944 | bytes 12582912 | tf_op jit(solution)/shard_map/qkv/pallas_call | solution.py:126
  214.9 29.6 %collective-permute-done.10.refs_0_ = bf16[256,4096]{1,0:T(8,128)(2,1)} collective-permute-done((bf16[256,4096]{1,0:T(8,128)(2,1)}, bf16[256,4096]{1,0:T(8,128)(2,1)}, u32[]{:S(2)}, u32[]{:S(2)}) %collective-permute-start.10) | collective-permute-done | bytes 2097184 | tf_op jit(solution)/shard_map/ppermute | solution.py:711
  249.9 7.9 qkv.10.refs_5_.refs_7_
  259.3 11.1 qkv.11.refs_14_.refs_2_
  270.4 22.9 %collective-permute-done.12.refs_8_ = bf16[8,2,256,256]{3,2,1,0:T(8,128)(2,1)} collective-permute-done((bf16[8,2,256,256]{3,2,1,0:T(8,128)(2,1)}, bf16[8,2,256,256]{3,2,1,0:T(8,128)(2,1)}, u32[]{:S(2)}, u32[]{:S(2)}) %collective-permute-start.12) | collective-permute-done | bytes 2097184 | tf_op jit(solution)/shard_map/ppermute | solution.py:711
  293.4 11.2 collective-permute-done.13.refs_9_
  304.9 10.9 collective-permute-done.14.refs_10_
  316.1 10.9 collective-permute-done.15.refs_11_
  327.1 10.8 collective-permute-done.16.refs_12_
  337.8 29.1 %flash.4 = (bf16[2,256,1024]{2,1,0:T(8,128)(2,1)}, bf16[2,256,1024]{2,1,0:T(8,128)(2,1)}, bf16[2,256,1024]{2,1,0:T(8,128)(2,1)}, bf16[2,256,1024]{2,1,0:T(8,128)(2,1)}, f32[8,128]{1,0:T(8,128)}) custom-call(s32[867]{0:T(1024)} %dynamic-slice_reduce_fusion.refs_0_, bf16[8,1024,256]{2,1,0:T(8,128)(2,1)} %get-tuple-element.79.refs_1_, ...), custom_call_target="tpu_custom_call" | custom-call | flops 27917287424 | bytes 8388608 | tf_op jit(solution)/shard_map/flash/pallas_call | solution.py:382
  367.9 43.9 %flash.5 = (bf16[2,256,1024]{2,1,0:T(8,128)(2,1)}, bf16[2,256,1024]{2,1,0:T(8,128)(2,1)}, bf16[2,256,1024]{2,1,0:T(8,128)(2,1)}, bf16[2,256,1024]{2,1,0:T(8,128)(2,1)}, f32[8,128]{1,0:T(8,128)}) custom-call(s32[867]{0:T(1024)} %dynamic-slice_reduce_fusion.refs_0_, ...), custom_call_target="tpu_custom_call", output_to_operand_aliasing={{0}: (14, {}), {1}: (15, {}), {2}: (16, {}), {3}: (17, {})} | custom-call | flops 32212254720 | bytes 8388608 | tf_op jit(solution)/shard_map/flash/pallas_call | solution.py:382
  411.8 8.8 collective-permute-start.18
  422.5 43.8 %flash.6 = (bf16[2,256,1024]{2,1,0:T(8,128)(2,1)}, bf16[2,256,1024]{2,1,0:T(8,128)(2,1)}, bf16[2,256,1024]{2,1,0:T(8,128)(2,1)}, bf16[2,256,1024]{2,1,0:T(8,128)(2,1)}, f32[8,128]{1,0:T(8,128)}) custom-call(s32[867]{0:T(1024)} %dynamic-slice_reduce_fusion.refs_0_, bf16[8,1024,256]{2,1,0:T(8,128)(2,1)} %get-tuple-element.79.refs_1_, ...), custom_call_target="tpu_custom_call" | custom-call | flops 32212254720 | bytes 8388608 | tf_op jit(solution)/shard_map/flash/pallas_call | solution.py:382
  482.3 29.0 %outp.2 = (bf16[256,4096]{1,0:T(8,128)(2,1)}, bf16[256,4096]{1,0:T(8,128)(2,1)}, bf16[256,4096]{1,0:T(8,128)(2,1)}, bf16[256,4096]{1,0:T(8,128)(2,1)}) custom-call(bf16[2,256,1024]{2,1,0:T(8,128)(2,1)} %get-tuple-element.96.refs_0_, bf16[2,256,1024]{2,1,0:T(8,128)(2,1)} %collective-permute-done.17.refs_1_, ...), custom_call_target="tpu_custom_call" | custom-call | flops 17179869184 | bytes 33554432 | tf_op jit(solution)/shard_map/outp/pallas_call | solution.py:491
  511.4 3.9 collective-permute-start.29
  515.3 43.8 %flash.7 = (bf16[2,256,1024]{2,1,0:T(8,128)(2,1)}, bf16[2,256,1024]{2,1,0:T(8,128)(2,1)}, bf16[2,256,1024]{2,1,0:T(8,128)(2,1)}, bf16[2,256,1024]{2,1,0:T(8,128)(2,1)}, f32[8,128]{1,0:T(8,128)}) custom-call(s32[867]{0:T(1024)} %dynamic-slice_reduce_fusion.refs_0_, ...), custom_call_target="tpu_custom_call", output_to_operand_aliasing={{0}: (14, {}), {1}: (15, {}), {2}: (16, {}), {3}: (17, {})} | custom-call | flops 32212254720 | bytes 8388608 | tf_op jit(solution)/shard_map/flash/pallas_call | solution.py:382
  561.8 4.5 collective-permute-done.31.refs_3_
  566.3 86.7 %mlp.5 = (bf16[512,4096]{1,0:T(8,128)(2,1)}, bf16[512,4096]{1,0:T(8,128)(2,1)}) custom-call(bf16[256,4096]{1,0:T(8,128)(2,1)} %get-tuple-element.110.refs_0_, bf16[256,4096]{1,0:T(8,128)(2,1)} %collective-permute-done.29.refs_1_, bf16[256,4096]{1,0:T(8,128)(2,1)} %collective-permute-done.30.refs_2_, bf16[256,4096]{1,0:T(8,128)(2,1)} %collective-permute-done.31.refs_3_, ...), custom_call_target="tpu_custom_call" | custom-call | flops 77309411328 | bytes 75497472 | tf_op jit(solution)/shard_map/mlp/pallas_call | solution.py:576
  656.8 45.2 %collective-permute-done.37.refs_1_ = bf16[256,4096]{1,0:T(8,128)(2,1)} collective-permute-done((bf16[256,4096]{1,0:T(8,128)(2,1)}, bf16[256,4096]{1,0:T(8,128)(2,1)}, u32[]{:S(2)}, u32[]{:S(2)}) %collective-permute-start.37) | collective-permute-done | bytes 2097184 | tf_op jit(solution)/shard_map/ppermute | solution.py:711
  702.5 22.0 %collective-permute-done.34.refs_2_ = bf16[2,256,1024]{2,1,0:T(8,128)(2,1)} collective-permute-done((bf16[2,256,1024]{2,1,0:T(8,128)(2,1)}, bf16[2,256,1024]{2,1,0:T(8,128)(2,1)}, u32[]{:S(2)}, u32[]{:S(2)}) %collective-permute-start.34) | collective-permute-done | bytes 1048608 | tf_op jit(solution)/shard_map/ppermute | solution.py:711
  724.4 21.3 %collective-permute-done.35.refs_3_ = bf16[2,256,1024]{2,1,0:T(8,128)(2,1)} collective-permute-done((bf16[2,256,1024]{2,1,0:T(8,128)(2,1)}, bf16[2,256,1024]{2,1,0:T(8,128)(2,1)}, u32[]{:S(2)}, u32[]{:S(2)}) %collective-permute-start.35) | collective-permute-done | bytes 1048608 | tf_op jit(solution)/shard_map/ppermute | solution.py:711
  745.7 29.1 %outp.3 = (bf16[256,4096]{1,0:T(8,128)(2,1)}, bf16[256,4096]{1,0:T(8,128)(2,1)}, bf16[256,4096]{1,0:T(8,128)(2,1)}, bf16[256,4096]{1,0:T(8,128)(2,1)}) custom-call(bf16[2,256,1024]{2,1,0:T(8,128)(2,1)} %get-tuple-element.120.refs_0_, bf16[2,256,1024]{2,1,0:T(8,128)(2,1)} %collective-permute-done.33.refs_1_, ...), custom_call_target="tpu_custom_call" | custom-call | flops 17179869184 | bytes 33554432 | tf_op jit(solution)/shard_map/outp/pallas_call | solution.py:491
  774.8 4.3 add_convert_fusion.2.refs_7_
  779.1 87.0 %mlp.6 = (bf16[512,4096]{1,0:T(8,128)(2,1)}, bf16[512,4096]{1,0:T(8,128)(2,1)}) custom-call(bf16[256,4096]{1,0:T(8,128)(2,1)} %get-tuple-element.126.refs_0_, bf16[256,4096]{1,0:T(8,128)(2,1)} %collective-permute-done.37.refs_1_, bf16[256,4096]{1,0:T(8,128)(2,1)} %collective-permute-done.38.refs_2_, bf16[256,4096]{1,0:T(8,128)(2,1)} %collective-permute-done.39.refs_3_, ...), custom_call_target="tpu_custom_call" | custom-call | flops 77309411328 | bytes 75497472 | tf_op jit(solution)/shard_map/mlp/pallas_call | solution.py:576
  868.6 46.8 %collective-permute-done.42.refs_1_ = bf16[256,4096]{1,0:T(8,128)(2,1)} collective-permute-done((bf16[256,4096]{1,0:T(8,128)(2,1)}, bf16[256,4096]{1,0:T(8,128)(2,1)}, u32[]{:S(2)}, u32[]{:S(2)}) %collective-permute-start.42) | collective-permute-done | bytes 2097184 | tf_op jit(solution)/shard_map/ppermute | solution.py:711
  915.4 44.1 %collective-permute-done.36.refs_2_ = bf16[256,4096]{1,0:T(8,128)(2,1)} collective-permute-done((bf16[256,4096]{1,0:T(8,128)(2,1)}, bf16[256,4096]{1,0:T(8,128)(2,1)}, u32[]{:S(2)}, u32[]{:S(2)}) %collective-permute-start.36) | collective-permute-done | bytes 2097184 | tf_op jit(solution)/shard_map/ppermute | solution.py:711
  959.4 5.6 zsum.5.refs_0_
  965.0 4.4 add_convert_fusion.1.refs_7_
  969.4 86.8 %mlp.7 = (bf16[512,4096]{1,0:T(8,128)(2,1)}, bf16[512,4096]{1,0:T(8,128)(2,1)}) custom-call(bf16[256,4096]{1,0:T(8,128)(2,1)} %get-tuple-element.132.refs_0_, bf16[256,4096]{1,0:T(8,128)(2,1)} %collective-permute-done.42.refs_1_, bf16[256,4096]{1,0:T(8,128)(2,1)} %collective-permute-done.43.refs_2_, bf16[256,4096]{1,0:T(8,128)(2,1)} %collective-permute-done.44.refs_3_, ...), custom_call_target="tpu_custom_call" | custom-call | flops 77309411328 | bytes 75497472 | tf_op jit(solution)/shard_map/mlp/pallas_call | solution.py:576
  1058.2 46.8 %collective-permute-done.47.refs_1_ = bf16[256,4096]{1,0:T(8,128)(2,1)} collective-permute-done((bf16[256,4096]{1,0:T(8,128)(2,1)}, bf16[256,4096]{1,0:T(8,128)(2,1)}, u32[]{:S(2)}, u32[]{:S(2)}) %collective-permute-start.47) | collective-permute-done | bytes 2097184 | tf_op jit(solution)/shard_map/ppermute | solution.py:711
  1105.0 44.4 %collective-permute-done.41.refs_3_ = bf16[256,4096]{1,0:T(8,128)(2,1)} collective-permute-done((bf16[256,4096]{1,0:T(8,128)(2,1)}, bf16[256,4096]{1,0:T(8,128)(2,1)}, u32[]{:S(2)}, u32[]{:S(2)}) %collective-permute-start.41) | collective-permute-done | bytes 2097184 | tf_op jit(solution)/shard_map/ppermute | solution.py:711
  1149.5 5.8 zsum.6.refs_0_
  1155.3 4.3 add_convert_fusion.refs_7_
  1161.3 48.0 %mlp.8 = (bf16[256,4096]{1,0:T(8,128)(2,1)}, bf16[256,4096]{1,0:T(8,128)(2,1)}) custom-call(bf16[256,4096]{1,0:T(8,128)(2,1)} %get-tuple-element.137.refs_0_, bf16[256,4096]{1,0:T(8,128)(2,1)} %collective-permute-done.47.refs_1_, bf16[256,4096]{1,0:T(8,128)(2,1)} %collective-permute-done.48.refs_2_, bf16[256,4096]{1,0:T(8,128)(2,1)} %collective-permute-done.49.refs_3_, ...), custom_call_target="tpu_custom_call" | custom-call | flops 38654705664 | bytes 75497472 | tf_op jit(solution)/shard_map/mlp/pallas_call | solution.py:576
  1209.4 5.6 zsum.7.refs_0_
  1217.8 47.9 %mlp.9 = (bf16[256,4096]{1,0:T(8,128)(2,1)}, bf16[256,4096]{1,0:T(8,128)(2,1)}) custom-call(bf16[256,4096]{1,0:T(8,128)(2,1)} %get-tuple-element.137.refs_0_, bf16[256,4096]{1,0:T(8,128)(2,1)} %collective-permute-done.47.refs_1_, bf16[256,4096]{1,0:T(8,128)(2,1)} %collective-permute-done.48.refs_2_, bf16[256,4096]{1,0:T(8,128)(2,1)} %collective-permute-done.49.refs_3_, ...), custom_call_target="tpu_custom_call" | custom-call | flops 38654705664 | bytes 75497472 | tf_op jit(solution)/shard_map/mlp/pallas_call | solution.py:576
  1266.6 3.7 collective-permute-done.52.refs_2_
  1274.5 18.2 %collective-permute-done.51.refs_3_ = bf16[128,4096]{1,0:T(8,128)(2,1)} collective-permute-done((bf16[128,4096]{1,0:T(8,128)(2,1)}, bf16[128,4096]{1,0:T(8,128)(2,1)}, u32[]{:S(2)}, u32[]{:S(2)}) %collective-permute-start.51) | collective-permute-done | bytes 1048608 | tf_op jit(solution)/shard_map/ppermute | solution.py:711
  1295.9 18.3 %collective-permute-done.53.refs_3_ = bf16[128,4096]{1,0:T(8,128)(2,1)} collective-permute-done((bf16[128,4096]{1,0:T(8,128)(2,1)}, bf16[128,4096]{1,0:T(8,128)(2,1)}, u32[]{:S(2)}, u32[]{:S(2)}) %collective-permute-start.53) | collective-permute-done | bytes 1048608 | tf_op jit(solution)/shard_map/ppermute | solution.py:711
  (108 shorter events, 84.2 us)
Async XLA Ops:
  4.8 73.1 %collective-permute-start.5 = (bf16[256,4096]{1,0:T(8,128)(2,1)}, bf16[256,4096]{1,0:T(8,128)(2,1)}, u32[]{:S(2)}, u32[]{:S(2)}) collective-permute-start(bf16[256,4096]{1,0:T(8,128)(2,1)} %norm.4.refs_2_.refs_0_), channel_id=1, source_target_pairs={{0,2},{1,3},{2,0},{3,1},{4,6},{5,7},{6,4},{7,5}} | collective-permute-start | bytes 6291464 | tf_op jit(solution)/shard_map/ppermute | solution.py:711
  8.1 30.1 %collective-permute-start = (bf16[256,4096]{1,0:T(8,128)(2,1)}, bf16[256,4096]{1,0:T(8,128)(2,1)}, u32[]{:S(2)}, u32[]{:S(2)}) collective-permute-start(bf16[256,4096]{1,0:T(8,128)(2,1)} %norm.4.refs_2_.refs_0_), channel_id=1, source_target_pairs={{0,1},{1,0},{2,3},{3,2},{4,5},{5,4},{6,7},{7,6}} | collective-permute-start | bytes 6291464 | tf_op jit(solution)/shard_map/ppermute | solution.py:711
  11.6 26.7 %collective-permute-start.1 = (bf16[256,4096]{1,0:T(8,128)(2,1)}, bf16[256,4096]{1,0:T(8,128)(2,1)}, u32[]{:S(2)}, u32[]{:S(2)}) collective-permute-start(bf16[256,4096]{1,0:T(8,128)(2,1)} %norm.5.refs_2_.refs_1_), channel_id=1, source_target_pairs={{0,1},{1,0},{2,3},{3,2},{4,5},{5,4},{6,7},{7,6}} | collective-permute-start | bytes 6291464 | tf_op jit(solution)/shard_map/ppermute | solution.py:711
  15.5 22.7 %collective-permute-start.2 = (bf16[256,4096]{1,0:T(8,128)(2,1)}, bf16[256,4096]{1,0:T(8,128)(2,1)}, u32[]{:S(2)}, u32[]{:S(2)}) collective-permute-start(bf16[256,4096]{1,0:T(8,128)(2,1)} %norm.6.refs_2_), channel_id=1, source_target_pairs={{0,1},{1,0},{2,3},{3,2},{4,5},{5,4},{6,7},{7,6}} | collective-permute-start | bytes 6291464 | tf_op jit(solution)/shard_map/ppermute | solution.py:711
  18.9 19.3 %collective-permute-start.3 = (bf16[256,4096]{1,0:T(8,128)(2,1)}, bf16[256,4096]{1,0:T(8,128)(2,1)}, u32[]{:S(2)}, u32[]{:S(2)}) collective-permute-start(bf16[256,4096]{1,0:T(8,128)(2,1)} %norm.7.refs_3_), channel_id=1, source_target_pairs={{0,1},{1,0},{2,3},{3,2},{4,5},{5,4},{6,7},{7,6}} | collective-permute-start | bytes 6291464 | tf_op jit(solution)/shard_map/ppermute | solution.py:711
  78.0 48.3 %collective-permute-start.4 = (bf16[256,4096]{1,0:T(8,128)(2,1)}, bf16[256,4096]{1,0:T(8,128)(2,1)}, u32[]{:S(2)}, u32[]{:S(2)}) collective-permute-start(bf16[256,4096]{1,0:T(8,128)(2,1)} %norm.5.refs_2_.refs_1_), channel_id=1, source_target_pairs={{0,2},{1,3},{2,0},{3,1},{4,6},{5,7},{6,4},{7,5}} | collective-permute-start | bytes 6291464 | tf_op jit(solution)/shard_map/ppermute | solution.py:711
  126.3 68.7 %collective-permute-start.8 = (bf16[256,4096]{1,0:T(8,128)(2,1)}, bf16[256,4096]{1,0:T(8,128)(2,1)}, u32[]{:S(2)}, u32[]{:S(2)}) collective-permute-start(bf16[256,4096]{1,0:T(8,128)(2,1)} %norm.6.refs_2_), channel_id=1, source_target_pairs={{0,2},{1,3},{2,0},{3,1},{4,6},{5,7},{6,4},{7,5}} | collective-permute-start | bytes 6291464 | tf_op jit(solution)/shard_map/ppermute | solution.py:711
  195.0 5.8 collective-permute-start.9
  196.7 47.9 %collective-permute-start.10 = (bf16[256,4096]{1,0:T(8,128)(2,1)}, bf16[256,4096]{1,0:T(8,128)(2,1)}, u32[]{:S(2)}, u32[]{:S(2)}) collective-permute-start(bf16[256,4096]{1,0:T(8,128)(2,1)} %norm.7.refs_3_), channel_id=1, source_target_pairs={{0,2},{1,3},{2,0},{3,1},{4,6},{5,7},{6,4},{7,5}} | collective-permute-start | bytes 6291464 | tf_op jit(solution)/shard_map/ppermute | solution.py:711
  244.5 48.8 %collective-permute-start.12 = (bf16[8,2,256,256]{3,2,1,0:T(8,128)(2,1)}, bf16[8,2,256,256]{3,2,1,0:T(8,128)(2,1)}, u32[]{:S(2)}, u32[]{:S(2)}) collective-permute-start(bf16[8,2,256,256]{3,2,1,0:T(8,128)(2,1)} %get-tuple-element.80.refs_5_.refs_3_), channel_id=1, source_target_pairs={{0,4},{4,0},{1,5},{5,1},{2,6},{6,2},{3,7},{7,3}} | collective-permute-start | bytes 6291464 | tf_op jit(solution)/shard_map/ppermute | solution.py:711
  247.4 57.2 %collective-permute-start.13 = (bf16[2,2,256,256]{3,2,1,0:T(8,128)(2,1)}, bf16[2,2,256,256]{3,2,1,0:T(8,128)(2,1)}, u32[]{:S(2)}, u32[]{:S(2)}) collective-permute-start(bf16[2,2,256,256]{3,2,1,0:T(8,128)(2,1)} %get-tuple-element.82.refs_5_.refs_4_), channel_id=1, source_target_pairs={{0,4},{4,0},{1,5},{5,1},{2,6},{6,2},{3,7},{7,3}} | collective-permute-start | bytes 1572872 | tf_op jit(solution)/shard_map/ppermute | solution.py:711
  247.9 68.0 %collective-permute-start.14 = (bf16[2,2,256,256]{3,2,1,0:T(8,128)(2,1)}, bf16[2,2,256,256]{3,2,1,0:T(8,128)(2,1)}, u32[]{:S(2)}, u32[]{:S(2)}) collective-permute-start(bf16[2,2,256,256]{3,2,1,0:T(8,128)(2,1)} %get-tuple-element.85.refs_6_.refs_5_), channel_id=1, source_target_pairs={{0,4},{4,0},{1,5},{5,1},{2,6},{6,2},{3,7},{7,3}} | collective-permute-start | bytes 1572872 | tf_op jit(solution)/shard_map/ppermute | solution.py:711
  249.4 77.7 %collective-permute-start.15 = (bf16[2,2,256,256]{3,2,1,0:T(8,128)(2,1)}, bf16[2,2,256,256]{3,2,1,0:T(8,128)(2,1)}, u32[]{:S(2)}, u32[]{:S(2)}) collective-permute-start(bf16[2,2,256,256]{3,2,1,0:T(8,128)(2,1)} %get-tuple-element.89.refs_5_.refs_6_), channel_id=1, source_target_pairs={{0,4},{4,0},{1,5},{5,1},{2,6},{6,2},{3,7},{7,3}} | collective-permute-start | bytes 1572872 | tf_op jit(solution)/shard_map/ppermute | solution.py:711
  257.8 80.1 %collective-permute-start.16 = (bf16[2,2,256,256]{3,2,1,0:T(8,128)(2,1)}, bf16[2,2,256,256]{3,2,1,0:T(8,128)(2,1)}, u32[]{:S(2)}, u32[]{:S(2)}) collective-permute-start(bf16[2,2,256,256]{3,2,1,0:T(8,128)(2,1)} %qkv.10.refs_5_.refs_7_), channel_id=1, source_target_pairs={{0,4},{4,0},{1,5},{5,1},{2,6},{6,2},{3,7},{7,3}} | collective-permute-start | bytes 1572872 | tf_op jit(solution)/shard_map/ppermute | solution.py:711
  293.4 182.9 %collective-permute-start.20 = (bf16[1024,4096]{1,0:T(8,128)(2,1)}, bf16[1024,4096]{1,0:T(8,128)(2,1)}, u32[]{:S(2)}, u32[]{:S(2)}) collective-permute-start(bf16[1024,4096]{1,0:T(8,128)(2,1)} %bitcast.24), channel_id=1, source_target_pairs={{0,1},{1,0},{2,3},{3,2},{4,5},{5,4},{6,7},{7,6}} | collective-permute-start | bytes 25165832 | tf_op jit(solution)/shard_map/ppermute | solution.py:711
  304.6 62.3 %collective-permute-start.21 = (bf16[256,4096]{1,0:T(8,128)(2,1)}, bf16[256,4096]{1,0:T(8,128)(2,1)}, u32[]{:S(2)}, u32[]{:S(2)}) collective-permute-start(bf16[256,4096]{1,0:T(8,128)(2,1)} %get-tuple-element.101), channel_id=1, source_target_pairs={{0,2},{1,3},{2,0},{3,1},{4,6},{5,7},{6,4},{7,5}} | collective-permute-start | bytes 6291464 | tf_op jit(solution)/shard_map/ppermute | solution.py:711
  315.8 96.0 %collective-permute-start.22 = (bf16[256,4096]{1,0:T(8,128)(2,1)}, bf16[256,4096]{1,0:T(8,128)(2,1)}, u32[]{:S(2)}, u32[]{:S(2)}) collective-permute-start(bf16[256,4096]{1,0:T(8,128)(2,1)} %get-tuple-element.103), channel_id=1, source_target_pairs={{0,2},{1,3},{2,0},{3,1},{4,6},{5,7},{6,4},{7,5}} | collective-permute-start | bytes 6291464 | tf_op jit(solution)/shard_map/ppermute | solution.py:711
  366.9 53.7 %collective-permute-start.23 = (bf16[256,4096]{1,0:T(8,128)(2,1)}, bf16[256,4096]{1,0:T(8,128)(2,1)}, u32[]{:S(2)}, u32[]{:S(2)}) collective-permute-start(bf16[256,4096]{1,0:T(8,128)(2,1)} %collective-permute-done.21.refs_6_), channel_id=1, source_target_pairs={{0,4},{4,0},{1,5},{5,1},{2,6},{6,2},{3,7},{7,3}} | collective-permute-start | bytes 6291464 | tf_op jit(solution)/shard_map/ppermute | solution.py:711
  411.8 57.0 %collective-permute-start.17 = (bf16[2,256,1024]{2,1,0:T(8,128)(2,1)}, bf16[2,256,1024]{2,1,0:T(8,128)(2,1)}, u32[]{:S(2)}, u32[]{:S(2)}) collective-permute-start(bf16[2,256,1024]{2,1,0:T(8,128)(2,1)} %get-tuple-element.97), channel_id=1, source_target_pairs={{0,1},{1,0},{2,3},{3,2},{4,5},{5,4},{6,7},{7,6}} | collective-permute-start | bytes 3145736 | tf_op jit(solution)/shard_map/ppermute | solution.py:711
  411.8 57.4 %collective-permute-start.18 = (bf16[2,256,1024]{2,1,0:T(8,128)(2,1)}, bf16[2,256,1024]{2,1,0:T(8,128)(2,1)}, u32[]{:S(2)}, u32[]{:S(2)}) collective-permute-start(bf16[2,256,1024]{2,1,0:T(8,128)(2,1)} %get-tuple-element.98), channel_id=1, source_target_pairs={{0,2},{1,3},{2,0},{3,1},{4,6},{5,7},{6,4},{7,5}} | collective-permute-start | bytes 3145736 | tf_op jit(solution)/shard_map/ppermute | solution.py:711
  420.6 48.7 %collective-permute-start.19 = (bf16[2,256,1024]{2,1,0:T(8,128)(2,1)}, bf16[2,256,1024]{2,1,0:T(8,128)(2,1)}, u32[]{:S(2)}, u32[]{:S(2)}) collective-permute-start(bf16[2,256,1024]{2,1,0:T(8,128)(2,1)} %get-tuple-element.99), channel_id=1, source_target_pairs={{0,3},{1,2},{2,1},{3,0},{4,7},{5,6},{6,5},{7,4}} | collective-permute-start | bytes 3145736 | tf_op jit(solution)/shard_map/ppermute | solution.py:711
  420.6 48.2 %collective-permute-start.24 = (bf16[256,4096]{1,0:T(8,128)(2,1)}, bf16[256,4096]{1,0:T(8,128)(2,1)}, u32[]{:S(2)}, u32[]{:S(2)}) collective-permute-start(bf16[256,4096]{1,0:T(8,128)(2,1)} %collective-permute-done.22.refs_7_), channel_id=1, source_target_pairs={{0,4},{4,0},{1,5},{5,1},{2,6},{6,2},{3,7},{7,3}} | collective-permute-start | bytes 6291464 | tf_op jit(solution)/shard_map/ppermute | solution.py:711
  468.8 7.5 collective-permute-start.26
  469.3 10.0 collective-permute-start.27
  469.3 13.0 collective-permute-start.28
  511.3 50.5 %collective-permute-start.30 = (bf16[256,4096]{1,0:T(8,128)(2,1)}, bf16[256,4096]{1,0:T(8,128)(2,1)}, u32[]{:S(2)}, u32[]{:S(2)}) collective-permute-start(bf16[256,4096]{1,0:T(8,128)(2,1)} %get-tuple-element.110.refs_0_), channel_id=1, source_target_pairs={{0,1},{1,0},{2,3},{3,2},{4,5},{5,4},{6,7},{7,6}} | collective-permute-start | bytes 6291464 | tf_op jit(solution)/shard_map/ppermute | solution.py:711
  511.4 50.3 %collective-permute-start.29 = (bf16[256,4096]{1,0:T(8,128)(2,1)}, bf16[256,4096]{1,0:T(8,128)(2,1)}, u32[]{:S(2)}, u32[]{:S(2)}) collective-permute-start(bf16[256,4096]{1,0:T(8,128)(2,1)} %get-tuple-element.110.refs_0_), channel_id=1, source_target_pairs={{0,2},{1,3},{2,0},{3,1},{4,6},{5,7},{6,4},{7,5}} | collective-permute-start | bytes 6291464 | tf_op jit(solution)/shard_map/ppermute | solution.py:711
  653.0 121.8 %collective-permute-start.32 = (bf16[512,4096]{1,0:T(8,128)(2,1)}, bf16[512,4096]{1,0:T(8,128)(2,1)}, u32[]{:S(2)}, u32[]{:S(2)}) collective-permute-start(bf16[512,4096]{1,0:T(8,128)(2,1)} %get-tuple-element.119), channel_id=1, source_target_pairs={{0,1},{1,0},{2,3},{3,2},{4,5},{5,4},{6,7},{7,6}} | collective-permute-start | bytes 12582920 | tf_op jit(solution)/shard_map/ppermute | solution.py:711
  653.1 48.8 %collective-permute-start.37 = (bf16[256,4096]{1,0:T(8,128)(2,1)}, bf16[256,4096]{1,0:T(8,128)(2,1)}, u32[]{:S(2)}, u32[]{:S(2)}) collective-permute-start(bf16[256,4096]{1,0:T(8,128)(2,1)} %get-tuple-element.126.refs_0_), channel_id=1, source_target_pairs={{0,2},{1,3},{2,0},{3,1},{4,6},{5,7},{6,4},{7,5}} | collective-permute-start | bytes 6291464 | tf_op jit(solution)/shard_map/ppermute | solution.py:711
  654.9 47.1 %collective-permute-start.33 = (bf16[2,256,1024]{2,1,0:T(8,128)(2,1)}, bf16[2,256,1024]{2,1,0:T(8,128)(2,1)}, u32[]{:S(2)}, u32[]{:S(2)}) collective-permute-start(bf16[2,256,1024]{2,1,0:T(8,128)(2,1)} %get-tuple-element.121), channel_id=1, source_target_pairs={{0,1},{1,0},{2,3},{3,2},{4,5},{5,4},{6,7},{7,6}} | collective-permute-start | bytes 3145736 | tf_op jit(solution)/shard_map/ppermute | solution.py:711
  655.0 69.5 %collective-permute-start.34 = (bf16[2,256,1024]{2,1,0:T(8,128)(2,1)}, bf16[2,256,1024]{2,1,0:T(8,128)(2,1)}, u32[]{:S(2)}, u32[]{:S(2)}) collective-permute-start(bf16[2,256,1024]{2,1,0:T(8,128)(2,1)} %get-tuple-element.122), channel_id=1, source_target_pairs={{0,2},{1,3},{2,0},{3,1},{4,6},{5,7},{6,4},{7,5}} | collective-permute-start | bytes 3145736 | tf_op jit(solution)/shard_map/ppermute | solution.py:711
  655.3 90.4 %collective-permute-start.35 = (bf16[2,256,1024]{2,1,0:T(8,128)(2,1)}, bf16[2,256,1024]{2,1,0:T(8,128)(2,1)}, u32[]{:S(2)}, u32[]{:S(2)}) collective-permute-start(bf16[2,256,1024]{2,1,0:T(8,128)(2,1)} %get-tuple-element.123), channel_id=1, source_target_pairs={{0,3},{1,2},{2,1},{3,0},{4,7},{5,6},{6,5},{7,4}} | collective-permute-start | bytes 3145736 | tf_op jit(solution)/shard_map/ppermute | solution.py:711
  702.0 77.2 %collective-permute-start.38 = (bf16[256,4096]{1,0:T(8,128)(2,1)}, bf16[256,4096]{1,0:T(8,128)(2,1)}, u32[]{:S(2)}, u32[]{:S(2)}) collective-permute-start(bf16[256,4096]{1,0:T(8,128)(2,1)} %get-tuple-element.126.refs_0_), channel_id=1, source_target_pairs={{0,1},{1,0},{2,3},{3,2},{4,5},{5,4},{6,7},{7,6}} | collective-permute-start | bytes 6291464 | tf_op jit(solution)/shard_map/ppermute | solution.py:711
  702.0 77.1 %collective-permute-start.39 = (bf16[256,4096]{1,0:T(8,128)(2,1)}, bf16[256,4096]{1,0:T(8,128)(2,1)}, u32[]{:S(2)}, u32[]{:S(2)}) collective-permute-start(bf16[256,4096]{1,0:T(8,128)(2,1)} %collective-permute-done.37.refs_1_), channel_id=1, source_target_pairs={{0,1},{1,0},{2,3},{3,2},{4,5},{5,4},{6,7},{7,6}} | collective-permute-start | bytes 6291464 | tf_op jit(solution)/shard_map/ppermute | solution.py:711
  866.1 98.9 %collective-permute-start.40 = (bf16[512,4096]{1,0:T(8,128)(2,1)}, bf16[512,4096]{1,0:T(8,128)(2,1)}, u32[]{:S(2)}, u32[]{:S(2)}) collective-permute-start(bf16[512,4096]{1,0:T(8,128)(2,1)} %get-tuple-element.129), channel_id=1, source_target_pairs={{0,1},{1,0},{2,3},{3,2},{4,5},{5,4},{6,7},{7,6}} | collective-permute-start | bytes 12582920 | tf_op jit(solution)/shard_map/ppermute | solution.py:711
  866.5 48.8 %collective-permute-start.42 = (bf16[256,4096]{1,0:T(8,128)(2,1)}, bf16[256,4096]{1,0:T(8,128)(2,1)}, u32[]{:S(2)}, u32[]{:S(2)}) collective-permute-start(bf16[256,4096]{1,0:T(8,128)(2,1)} %get-tuple-element.132.refs_0_), channel_id=1, source_target_pairs={{0,2},{1,3},{2,0},{3,1},{4,6},{5,7},{6,4},{7,5}} | collective-permute-start | bytes 6291464 | tf_op jit(solution)/shard_map/ppermute | solution.py:711
  868.3 91.2 %collective-permute-start.36 = (bf16[256,4096]{1,0:T(8,128)(2,1)}, bf16[256,4096]{1,0:T(8,128)(2,1)}, u32[]{:S(2)}, u32[]{:S(2)}) collective-permute-start(bf16[256,4096]{1,0:T(8,128)(2,1)} %add_convert_fusion.2.refs_7_), channel_id=1, source_target_pairs={{0,2},{1,3},{2,0},{3,1},{4,6},{5,7},{6,4},{7,5}} | collective-permute-start | bytes 6291464 | tf_op jit(solution)/shard_map/ppermute | solution.py:711
  868.6 100.8 %collective-permute-start.43 = (bf16[256,4096]{1,0:T(8,128)(2,1)}, bf16[256,4096]{1,0:T(8,128)(2,1)}, u32[]{:S(2)}, u32[]{:S(2)}) collective-permute-start(bf16[256,4096]{1,0:T(8,128)(2,1)} %get-tuple-element.132.refs_0_), channel_id=1, source_target_pairs={{0,1},{1,0},{2,3},{3,2},{4,5},{5,4},{6,7},{7,6}} | collective-permute-start | bytes 6291464 | tf_op jit(solution)/shard_map/ppermute | solution.py:711
  915.3 54.0 %collective-permute-start.44 = (bf16[256,4096]{1,0:T(8,128)(2,1)}, bf16[256,4096]{1,0:T(8,128)(2,1)}, u32[]{:S(2)}, u32[]{:S(2)}) collective-permute-start(bf16[256,4096]{1,0:T(8,128)(2,1)} %collective-permute-done.42.refs_1_), channel_id=1, source_target_pairs={{0,1},{1,0},{2,3},{3,2},{4,5},{5,4},{6,7},{7,6}} | collective-permute-start | bytes 6291464 | tf_op jit(solution)/shard_map/ppermute | solution.py:711
  1056.1 99.1 %collective-permute-start.45 = (bf16[512,4096]{1,0:T(8,128)(2,1)}, bf16[512,4096]{1,0:T(8,128)(2,1)}, u32[]{:S(2)}, u32[]{:S(2)}) collective-permute-start(bf16[512,4096]{1,0:T(8,128)(2,1)} %get-tuple-element.135), channel_id=1, source_target_pairs={{0,1},{1,0},{2,3},{3,2},{4,5},{5,4},{6,7},{7,6}} | collective-permute-start | bytes 12582920 | tf_op jit(solution)/shard_map/ppermute | solution.py:711
  1056.2 48.8 %collective-permute-start.47 = (bf16[256,4096]{1,0:T(8,128)(2,1)}, bf16[256,4096]{1,0:T(8,128)(2,1)}, u32[]{:S(2)}, u32[]{:S(2)}) collective-permute-start(bf16[256,4096]{1,0:T(8,128)(2,1)} %get-tuple-element.137.refs_0_), channel_id=1, source_target_pairs={{0,2},{1,3},{2,0},{3,1},{4,6},{5,7},{6,4},{7,5}} | collective-permute-start | bytes 6291464 | tf_op jit(solution)/shard_map/ppermute | solution.py:711
  1057.9 91.5 %collective-permute-start.41 = (bf16[256,4096]{1,0:T(8,128)(2,1)}, bf16[256,4096]{1,0:T(8,128)(2,1)}, u32[]{:S(2)}, u32[]{:S(2)}) collective-permute-start(bf16[256,4096]{1,0:T(8,128)(2,1)} %add_convert_fusion.1.refs_7_), channel_id=1, source_target_pairs={{0,2},{1,3},{2,0},{3,1},{4,6},{5,7},{6,4},{7,5}} | collective-permute-start | bytes 6291464 | tf_op jit(solution)/shard_map/ppermute | solution.py:711
  1058.2 103.1 %collective-permute-start.48 = (bf16[256,4096]{1,0:T(8,128)(2,1)}, bf16[256,4096]{1,0:T(8,128)(2,1)}, u32[]{:S(2)}, u32[]{:S(2)}) collective-permute-start(bf16[256,4096]{1,0:T(8,128)(2,1)} %get-tuple-element.137.refs_0_), channel_id=1, source_target_pairs={{0,1},{1,0},{2,3},{3,2},{4,5},{5,4},{6,7},{7,6}} | collective-permute-start | bytes 6291464 | tf_op jit(solution)/shard_map/ppermute | solution.py:711
  1105.0 56.3 %collective-permute-start.49 = (bf16[256,4096]{1,0:T(8,128)(2,1)}, bf16[256,4096]{1,0:T(8,128)(2,1)}, u32[]{:S(2)}, u32[]{:S(2)}) collective-permute-start(bf16[256,4096]{1,0:T(8,128)(2,1)} %collective-permute-done.47.refs_1_), channel_id=1, source_target_pairs={{0,1},{1,0},{2,3},{3,2},{4,5},{5,4},{6,7},{7,6}} | collective-permute-start | bytes 6291464 | tf_op jit(solution)/shard_map/ppermute | solution.py:711
  1159.6 49.8 %collective-permute-start.46 = (bf16[256,4096]{1,0:T(8,128)(2,1)}, bf16[256,4096]{1,0:T(8,128)(2,1)}, u32[]{:S(2)}, u32[]{:S(2)}) collective-permute-start(bf16[256,4096]{1,0:T(8,128)(2,1)} %add_convert_fusion.refs_7_), channel_id=1, source_target_pairs={{0,2},{1,3},{2,0},{3,1},{4,6},{5,7},{6,4},{7,5}} | collective-permute-start | bytes 6291464 | tf_op jit(solution)/shard_map/ppermute | solution.py:711
  1209.4 5.6 collective-permute-start.50
  1266.3 26.3 %collective-permute-start.51 = (bf16[128,4096]{1,0:T(8,128)(2,1)}, bf16[128,4096]{1,0:T(8,128)(2,1)}, u32[]{:S(2)}, u32[]{:S(2)}) collective-permute-start(bf16[128,4096]{1,0:T(8,128)(2,1)} %add_convert_fusion.4.refs_7_), channel_id=1, source_target_pairs={{0,2},{1,3},{2,0},{3,1},{4,6},{5,7},{6,4},{7,5}} | collective-permute-start | bytes 3145736 | tf_op jit(solution)/shard_map/ppermute | solution.py:711
  1274.1 40.0 %collective-permute-start.53 = (bf16[128,4096]{1,0:T(8,128)(2,1)}, bf16[128,4096]{1,0:T(8,128)(2,1)}, u32[]{:S(2)}, u32[]{:S(2)}) collective-permute-start(bf16[128,4096]{1,0:T(8,128)(2,1)} %add_convert_fusion.3.refs_5_), channel_id=1, source_target_pairs={{0,2},{1,3},{2,0},{3,1},{4,6},{5,7},{6,4},{7,5}} | collective-permute-start | bytes 3145736 | tf_op jit(solution)/shard_map/ppermute | solution.py:711
  (9 other events, 36.0 us)

commit v10 on v9

--- a/solution.py
+++ b/solution.py
@@ -408,7 +408,8 @@
     )(tab, *qs, *kvs, *sts, *more, *after)
 
 
-def out_kernel(*refs, blocks, n_w, n_run, at):
+def out_kernel(*refs, blocks, n_w, runs):
+    n_run = len(runs)
     n_o, n_out = 4, 2 * n_run
     o_refs, w_refs, x_ref, g_ref = refs[:n_o], refs[n_o:n_o + n_w], refs[n_o + n_w], refs[n_o + n_w + 1]
     outs = refs[n_o + n_w + 2:n_o + n_w + 2 + n_out]
@@ -440,7 +441,6 @@
                     loads[2 * k + p].append((src.at[:, pl.ds(pl.multiple_of(part * half, half), half)],
                                              o_scr.at[rows, pl.ds(k * width + p * half, half)]))
     copies = [[pltpu.make_async_copy(src, dst, o_sem.at[k, i]) for i, (src, dst) in enumerate(ls)] for k, ls in enumerate(loads)]
-    x_copy = pltpu.make_async_copy(x_ref.at[pl.ds(at * n_run * RUN, n_run * RUN), :], x_scr, x_sem)
     for cp in copies[0]:
         cp.start()
     for i in range(n_slots - 1):
@@ -448,7 +448,8 @@
     for ls in copies[1:]:
         for cp in ls:
             cp.start()
-    x_copy.start()
+    for i, run in enumerate(runs):
+        pltpu.make_async_copy(x_ref.at[pl.ds(run * RUN, RUN), :], x_scr.at[pl.ds(i * RUN, RUN), :], x_sem).start()
     acc_scr[...] = jnp.zeros_like(acc_scr)
 
     def one(k, carry):
@@ -465,7 +466,7 @@
         return carry
 
     lax.fori_loop(0, len(blocks), one, 0)
-    x_copy.wait()
+    pltpu.make_async_copy(x_scr, x_scr, x_sem).wait()
 
     def rows32(r, carry):
         rows = pl.ds(pl.multiple_of(r * 32, 32), 32)
@@ -484,12 +485,12 @@
         cp.wait()
 
 
-def out_proj(os, ws, blocks, x_rows, gain, at, after=()):
+def out_proj(os, ws, blocks, x_rows, gain, runs, after=()):
     dim = x_rows.shape[1]
     n_run, _, width = os[0].shape
     rows = n_run * RUN
     return pl.pallas_call(
-        ordered(functools.partial(out_kernel, blocks=blocks, n_w=len(ws), n_run=n_run, at=at),
+        ordered(functools.partial(out_kernel, blocks=blocks, n_w=len(ws), runs=runs),
                 len(os) + len(ws) + 2, after),
         grid=(1,),
         in_specs=[ANY] * (len(os) + len(ws) + 1) + [pl.BlockSpec((1, dim), lambda i: (0, 0))] + [ANY] * len(after),
@@ -650,7 +651,7 @@
 
 def work_tables(cps, piece):
     per = piece // 2 // RUN
-    early = 2 * per + 2
+    early = 3 * per
     stage = lambda r: 0 if r < early else 1
     calls = [(0, list(range(early)))]
     calls += [(1, [j, per + j, 2 * per + 2 * j, 2 * per + 2 * j + 1]) for j in range(per)]
@@ -743,9 +744,9 @@
         rows = half // n_piece
         wo_c = send(over_core, tied(wo, kvs[-1]))
 
-        tiles = [(0, i) for i in range(2 * n_run)] + [(1, 0), (1, 1)]
-        st, *wo_x = flash(tab, [q_here, q_far[0]], tiles, kvs[:2], base=bases[0], work=int(work[0]), cut=wo,
-                         n_cut=n_piece, after=(kvs[-1],))
+        tiles = [(0, i) for i in range(2 * n_run)] + [(a, i) for a in (1, 2) for i in range(2)]
+        st, *wo_x = flash(tab, [q_here, *q_far], tiles, kvs, base=bases[0], work=int(work[0]), cut=wo,
+                         n_cut=n_piece)
         wo_x = [send(over_x, w) for w in wo_x]
         far_qkv(3, far_qkv(2, st))
         kvs = kvs + [send(over_y, kv) for kv in kvs]
@@ -762,10 +763,13 @@
             here = tied(wo_a[p], prev)
             wo_yb[p] = (here, send(over_core, here))
 
-        def attend(j):
+        order = (0, 3, 1, 2)
+
+        def attend(at):
+            j = order[at]
             held = 2 * n_run + 2 * j
-            carried = [j, n_run + j] + ([held, held + 1] if j == 0 else [None, None])
-            pair = j % 2
+            carried = [j, n_run + j] + ([held, held + 1] if held < len(tiles) else [None, None])
+            pair = at % 2
             *o, done = flash(
                 tab, [q_here, q_far[j]], [(0, j), (0, n_run + j), (1, 0), (1, 1)], kvs,
                 base=bases[1 + j], work=int(work[1 + j]), st=st, st_src=carried, old=os.pop() if pair else None, slots=2,
@@ -782,7 +786,7 @@
                 for held in (wo_ya, wo_yb):
                     blocks.append([(len(ws) + p, 0, rows) for p in range(n_piece)])
                     ws += [held[p][k] for p in range(n_piece)]
-            got = out_proj(os[i], ws, blocks, x_rows, gm, i, after=(prev,))
+            got = out_proj(os[i], ws, blocks, x_rows, gm, order[2 * i:2 * i + 2], after=(prev,))
             for y, b in zip(got[::2], got[1::2]):
                 outs.append((y, b, send(over_x, b), send(over_core, b)))
             return got[0]
@@ -807,7 +811,7 @@
 
         def finish(c):
             j, first, size = chunks[c]
-            return sum_rows(z, *sums[c], outs[j][0], first, size, j * RUN + first, n_run * RUN,
+            return sum_rows(z, *sums[c], outs[j][0], first, size, order[j] * RUN + first, n_run * RUN,
                         after=() if prev is z else (prev,))
 
         relay_b(0)

time: 1330 us -> 1340 us (level)
  transfers between devices with their start and end apart: 54 -> 54, of which waited for: 27 -> 28; matrix products, arithmetic and copies ran while one was open for 3% -> 3% of each run, Pallas kernels for 32% -> 32%
where the time goes in v10:
time: 1340 us; the launch traced here: 1330 us
  Pallas kernels  764 us (57%)
  waiting for transfers between devices  482 us (36%)
  starting transfers between devices  40.3 us (3%)
  other arithmetic  23.1 us (2%)
  local copies, waits for them, and re-layouts  19.2 us (1%)
    ppermute x54, waiting for transfers between devices, send(): return lax.ppermute(v, *axis_pairs)  482 us
    pallas_call x5, Pallas kernels, mlp(): pl.pallas_call(ordered(functools.partial(mlp_kernel, n_in=len(bs), first=...  356 us
    pallas_call x5, Pallas kernels, flash(): pl.pallas_call(ordered(functools.partial(flash_kernel, q_src=q_src, kv_sr...  211 us
    pallas_call x6, Pallas kernels, qkv(): pl.pallas_call(ordered(functools.partial(qkv_kernel, n_in=n_in, n_q=n_q,...  101 us
    pallas_call x2, Pallas kernels, out_proj(): pl.pallas_call(ordered(functools.partial(out_kernel, blocks=blocks, n_w=l...  58.1 us
    ppermute x54, starting transfers between devices, send(): return lax.ppermute(v, *axis_pairs)  40.3 us
  transfers between devices with their start and end apart: 54, of which 28 were waited for; matrix products, arithmetic and copies ran while one was open for 3% of the time, Pallas kernels for 32%

profile of v10, /device:TPU:0, one launch (start us, length us, event | category | flops | bytes accessed | tf_op | source)
XLA Modules:
  0.0 1329.4 jit_solution(7776913728940484772)
XLA Ops:
  20.1 9.3 bitcast_dynamic-update-slice_fusion
  29.5 4.8 multiply_sine_fusion
  38.2 39.7 %qkv.6 = (bf16[8,1024,256]{2,1,0:T(8,128)(2,1)}, bf16[8,2,256,256]{3,2,1,0:T(8,128)(2,1)}) custom-call(bf16[256,4096]{1,0:T(8,128)(2,1)} %norm.4.refs_2_.refs_0_, bf16[256,4096]{1,0:T(8,128)(2,1)} %norm.5.refs_2_.refs_1_, bf16[256,4096]{1,0:T(8,128)(2,1)} %norm.6.refs_2_, bf16[256,4096]{1,0:T(8,128)(2,1)} %norm.7.refs_3_, ...), custom_call_target="tpu_custom_call" | custom-call | flops 25769803776 | bytes 12582912 | tf_op jit(solution)/shard_map/qkv/pallas_call | solution.py:126
  77.9 4.5 collective-permute-done.7.refs_1_
  82.4 14.1 %qkv.7 = (bf16[2,1024,256]{2,1,0:T(8,128)(2,1)}, bf16[2,2,256,256]{3,2,1,0:T(8,128)(2,1)}) custom-call(bf16[256,4096]{1,0:T(8,128)(2,1)} %collective-permute-done.6.refs_0_, bf16[256,4096]{1,0:T(8,128)(2,1)} %collective-permute-done.7.refs_1_, bf16[4096,1536]{1,0:T(8,128)(2,1)} %bitcast_dynamic-update-slice_fusion.1.refs_8_.refs_2_, ...), custom_call_target="tpu_custom_call" | custom-call | flops 6442450944 | bytes 12582912 | tf_op jit(solution)/shard_map/qkv/pallas_call | solution.py:126
  96.5 29.7 %collective-permute-done.8.refs_0_ = bf16[256,4096]{1,0:T(8,128)(2,1)} collective-permute-done((bf16[256,4096]{1,0:T(8,128)(2,1)}, bf16[256,4096]{1,0:T(8,128)(2,1)}, u32[]{:S(2)}, u32[]{:S(2)}) %collective-permute-start.8) | collective-permute-done | bytes 2097184 | tf_op jit(solution)/shard_map/ppermute | solution.py:712
  130.7 14.3 %qkv.8 = (bf16[2,1024,256]{2,1,0:T(8,128)(2,1)}, bf16[2,2,256,256]{3,2,1,0:T(8,128)(2,1)}) custom-call(bf16[256,4096]{1,0:T(8,128)(2,1)} %collective-permute-done.8.refs_0_, bf16[256,4096]{1,0:T(8,128)(2,1)} %collective-permute-done.9.refs_1_, bf16[4096,1536]{1,0:T(8,128)(2,1)} %bitcast_dynamic-update-slice_fusion.1.refs_8_.refs_2_, ...), custom_call_target="tpu_custom_call" | custom-call | flops 6442450944 | bytes 12582912 | tf_op jit(solution)/shard_map/qkv/pallas_call | solution.py:126
  145.1 64.5 %flash_part.1 = (f32[12,2,4,144,256]{4,3,2,1,0:T(8,128)}, bf16[256,4096]{1,0:T(8,128)(2,1)}, bf16[256,4096]{1,0:T(8,128)(2,1)}) custom-call(s32[869]{0:T(1024)} %dynamic-slice_reduce_fusion.refs_0_, bf16[8,1024,256]{2,1,0:T(8,128)(2,1)} %get-tuple-element.79.refs_1_, bf16[2,1024,256]{2,1,0:T(8,128)(2,1)} %get-tuple-element.82.refs_2_, ...), custom_call_target="tpu_custom_call" | custom-call | flops 51539607552 | bytes 3145728 | tf_op jit(solution)/shard_map/flash_part/pallas_call | solution.py:382
  215.4 14.1 %qkv.9 = (bf16[2,1024,256]{2,1,0:T(8,128)(2,1)}, bf16[2,2,256,256]{3,2,1,0:T(8,128)(2,1)}) custom-call(bf16[256,4096]{1,0:T(8,128)(2,1)} %collective-permute-done.5.refs_0_, bf16[256,4096]{1,0:T(8,128)(2,1)} %collective-permute-done.10.refs_1_, bf16[4096,1536]{1,0:T(8,128)(2,1)} %bitcast_dynamic-update-slice_fusion.1.refs_8_.refs_2_, ...), custom_call_target="tpu_custom_call" | custom-call | flops 6442450944 | bytes 12582912 | tf_op jit(solution)/shard_map/qkv/pallas_call | solution.py:126
  229.5 29.7 %collective-permute-done.4.refs_0_ = bf16[256,4096]{1,0:T(8,128)(2,1)} collective-permute-done((bf16[256,4096]{1,0:T(8,128)(2,1)}, bf16[256,4096]{1,0:T(8,128)(2,1)}, u32[]{:S(2)}, u32[]{:S(2)}) %collective-permute-start.4) | collective-permute-done | bytes 2097184 | tf_op jit(solution)/shard_map/ppermute | solution.py:712
  264.5 7.9 qkv.10.refs_5_.refs_7_
  274.0 11.1 qkv.11.refs_14_.refs_2_
  285.2 22.8 %collective-permute-done.12.refs_8_ = bf16[8,2,256,256]{3,2,1,0:T(8,128)(2,1)} collective-permute-done((bf16[8,2,256,256]{3,2,1,0:T(8,128)(2,1)}, bf16[8,2,256,256]{3,2,1,0:T(8,128)(2,1)}, u32[]{:S(2)}, u32[]{:S(2)}) %collective-permute-start.12) | collective-permute-done | bytes 2097184 | tf_op jit(solution)/shard_map/ppermute | solution.py:712
  308.0 11.2 collective-permute-done.13.refs_9_
  320.8 9.6 collective-permute-done.14.refs_10_
  332.0 9.6 collective-permute-done.15.refs_11_
  341.7 10.8 collective-permute-done.16.refs_12_
  352.5 29.1 %flash.4 = (bf16[2,256,1024]{2,1,0:T(8,128)(2,1)}, bf16[2,256,1024]{2,1,0:T(8,128)(2,1)}, bf16[2,256,1024]{2,1,0:T(8,128)(2,1)}, bf16[2,256,1024]{2,1,0:T(8,128)(2,1)}, f32[8,128]{1,0:T(8,128)}) custom-call(s32[869]{0:T(1024)} %dynamic-slice_reduce_fusion.refs_0_, bf16[8,1024,256]{2,1,0:T(8,128)(2,1)} %get-tuple-element.79.refs_1_, ...), custom_call_target="tpu_custom_call" | custom-call | flops 23622320128 | bytes 8388608 | tf_op jit(solution)/shard_map/flash/pallas_call | solution.py:382
  382.6 44.3 %flash.5 = (bf16[2,256,1024]{2,1,0:T(8,128)(2,1)}, bf16[2,256,1024]{2,1,0:T(8,128)(2,1)}, bf16[2,256,1024]{2,1,0:T(8,128)(2,1)}, bf16[2,256,1024]{2,1,0:T(8,128)(2,1)}, f32[8,128]{1,0:T(8,128)}) custom-call(s32[869]{0:T(1024)} %dynamic-slice_reduce_fusion.refs_0_, ...), custom_call_target="tpu_custom_call", output_to_operand_aliasing={{0}: (14, {}), {1}: (15, {}), {2}: (16, {}), {3}: (17, {})} | custom-call | flops 32212254720 | bytes 8388608 | tf_op jit(solution)/shard_map/flash/pallas_call | solution.py:382
  430.1 29.1 %flash.6 = (bf16[2,256,1024]{2,1,0:T(8,128)(2,1)}, bf16[2,256,1024]{2,1,0:T(8,128)(2,1)}, bf16[2,256,1024]{2,1,0:T(8,128)(2,1)}, bf16[2,256,1024]{2,1,0:T(8,128)(2,1)}, f32[8,128]{1,0:T(8,128)}) custom-call(s32[869]{0:T(1024)} %dynamic-slice_reduce_fusion.refs_0_, bf16[8,1024,256]{2,1,0:T(8,128)(2,1)} %get-tuple-element.79.refs_1_, ...), custom_call_target="tpu_custom_call" | custom-call | flops 23622320128 | bytes 8388608 | tf_op jit(solution)/shard_map/flash/pallas_call | solution.py:382
  459.2 17.8 %collective-permute-done.24.refs_9_ = bf16[256,4096]{1,0:T(8,128)(2,1)} collective-permute-done((bf16[256,4096]{1,0:T(8,128)(2,1)}, bf16[256,4096]{1,0:T(8,128)(2,1)}, u32[]{:S(2)}, u32[]{:S(2)}) %collective-permute-start.24) | collective-permute-done | bytes 2097184 | tf_op jit(solution)/shard_map/ppermute | solution.py:712
  478.0 3.5 collective-permute-done.25.refs_10_
  490.4 29.0 %outp.2 = (bf16[256,4096]{1,0:T(8,128)(2,1)}, bf16[256,4096]{1,0:T(8,128)(2,1)}, bf16[256,4096]{1,0:T(8,128)(2,1)}, bf16[256,4096]{1,0:T(8,128)(2,1)}) custom-call(bf16[2,256,1024]{2,1,0:T(8,128)(2,1)} %get-tuple-element.96.refs_0_, bf16[2,256,1024]{2,1,0:T(8,128)(2,1)} %collective-permute-done.17.refs_1_, ...), custom_call_target="tpu_custom_call" | custom-call | flops 17179869184 | bytes 33554432 | tf_op jit(solution)/shard_map/outp/pallas_call | solution.py:492
  519.7 7.3 collective-permute-start.29
  526.9 44.0 %flash.7 = (bf16[2,256,1024]{2,1,0:T(8,128)(2,1)}, bf16[2,256,1024]{2,1,0:T(8,128)(2,1)}, bf16[2,256,1024]{2,1,0:T(8,128)(2,1)}, bf16[2,256,1024]{2,1,0:T(8,128)(2,1)}, f32[8,128]{1,0:T(8,128)}) custom-call(s32[869]{0:T(1024)} %dynamic-slice_reduce_fusion.refs_0_, ...), custom_call_target="tpu_custom_call", output_to_operand_aliasing={{0}: (14, {}), {1}: (15, {}), {2}: (16, {}), {3}: (17, {})} | custom-call | flops 32212254720 | bytes 8388608 | tf_op jit(solution)/shard_map/flash/pallas_call | solution.py:382
  573.4 4.5 collective-permute-done.31.refs_3_
  577.9 86.7 %mlp.5 = (bf16[512,4096]{1,0:T(8,128)(2,1)}, bf16[512,4096]{1,0:T(8,128)(2,1)}) custom-call(bf16[256,4096]{1,0:T(8,128)(2,1)} %get-tuple-element.109.refs_0_, bf16[256,4096]{1,0:T(8,128)(2,1)} %collective-permute-done.29.refs_1_, bf16[256,4096]{1,0:T(8,128)(2,1)} %collective-permute-done.30.refs_2_, bf16[256,4096]{1,0:T(8,128)(2,1)} %collective-permute-done.31.refs_3_, ...), custom_call_target="tpu_custom_call" | custom-call | flops 77309411328 | bytes 75497472 | tf_op jit(solution)/shard_map/mlp/pallas_call | solution.py:577
  668.4 45.2 %collective-permute-done.37.refs_1_ = bf16[256,4096]{1,0:T(8,128)(2,1)} collective-permute-done((bf16[256,4096]{1,0:T(8,128)(2,1)}, bf16[256,4096]{1,0:T(8,128)(2,1)}, u32[]{:S(2)}, u32[]{:S(2)}) %collective-permute-start.37) | collective-permute-done | bytes 2097184 | tf_op jit(solution)/shard_map/ppermute | solution.py:712
  714.1 22.0 %collective-permute-done.34.refs_2_ = bf16[2,256,1024]{2,1,0:T(8,128)(2,1)} collective-permute-done((bf16[2,256,1024]{2,1,0:T(8,128)(2,1)}, bf16[2,256,1024]{2,1,0:T(8,128)(2,1)}, u32[]{:S(2)}, u32[]{:S(2)}) %collective-permute-start.34) | collective-permute-done | bytes 1048608 | tf_op jit(solution)/shard_map/ppermute | solution.py:712
  736.1 21.3 %collective-permute-done.35.refs_3_ = bf16[2,256,1024]{2,1,0:T(8,128)(2,1)} collective-permute-done((bf16[2,256,1024]{2,1,0:T(8,128)(2,1)}, bf16[2,256,1024]{2,1,0:T(8,128)(2,1)}, u32[]{:S(2)}, u32[]{:S(2)}) %collective-permute-start.35) | collective-permute-done | bytes 1048608 | tf_op jit(solution)/shard_map/ppermute | solution.py:712
  757.4 29.0 %outp.3 = (bf16[256,4096]{1,0:T(8,128)(2,1)}, bf16[256,4096]{1,0:T(8,128)(2,1)}, bf16[256,4096]{1,0:T(8,128)(2,1)}, bf16[256,4096]{1,0:T(8,128)(2,1)}) custom-call(bf16[2,256,1024]{2,1,0:T(8,128)(2,1)} %get-tuple-element.120.refs_0_, bf16[2,256,1024]{2,1,0:T(8,128)(2,1)} %collective-permute-done.33.refs_1_, ...), custom_call_target="tpu_custom_call" | custom-call | flops 17179869184 | bytes 33554432 | tf_op jit(solution)/shard_map/outp/pallas_call | solution.py:492
  786.4 4.3 add_convert_fusion.2.refs_7_
  790.7 87.0 %mlp.6 = (bf16[512,4096]{1,0:T(8,128)(2,1)}, bf16[512,4096]{1,0:T(8,128)(2,1)}) custom-call(bf16[256,4096]{1,0:T(8,128)(2,1)} %get-tuple-element.126.refs_0_, bf16[256,4096]{1,0:T(8,128)(2,1)} %collective-permute-done.37.refs_1_, bf16[256,4096]{1,0:T(8,128)(2,1)} %collective-permute-done.38.refs_2_, bf16[256,4096]{1,0:T(8,128)(2,1)} %collective-permute-done.39.refs_3_, ...), custom_call_target="tpu_custom_call" | custom-call | flops 77309411328 | bytes 75497472 | tf_op jit(solution)/shard_map/mlp/pallas_call | solution.py:577
  880.2 46.8 %collective-permute-done.42.refs_1_ = bf16[256,4096]{1,0:T(8,128)(2,1)} collective-permute-done((bf16[256,4096]{1,0:T(8,128)(2,1)}, bf16[256,4096]{1,0:T(8,128)(2,1)}, u32[]{:S(2)}, u32[]{:S(2)}) %collective-permute-start.42) | collective-permute-done | bytes 2097184 | tf_op jit(solution)/shard_map/ppermute | solution.py:712
  927.0 44.1 %collective-permute-done.36.refs_2_ = bf16[256,4096]{1,0:T(8,128)(2,1)} collective-permute-done((bf16[256,4096]{1,0:T(8,128)(2,1)}, bf16[256,4096]{1,0:T(8,128)(2,1)}, u32[]{:S(2)}, u32[]{:S(2)}) %collective-permute-start.36) | collective-permute-done | bytes 2097184 | tf_op jit(solution)/shard_map/ppermute | solution.py:712
  971.1 5.6 zsum.5.refs_0_
  976.6 4.3 add_convert_fusion.1.refs_7_
  981.0 86.8 %mlp.7 = (bf16[512,4096]{1,0:T(8,128)(2,1)}, bf16[512,4096]{1,0:T(8,128)(2,1)}) custom-call(bf16[256,4096]{1,0:T(8,128)(2,1)} %get-tuple-element.132.refs_0_, bf16[256,4096]{1,0:T(8,128)(2,1)} %collective-permute-done.42.refs_1_, bf16[256,4096]{1,0:T(8,128)(2,1)} %collective-permute-done.43.refs_2_, bf16[256,4096]{1,0:T(8,128)(2,1)} %collective-permute-done.44.refs_3_, ...), custom_call_target="tpu_custom_call" | custom-call | flops 77309411328 | bytes 75497472 | tf_op jit(solution)/shard_map/mlp/pallas_call | solution.py:577
  1069.9 46.8 %collective-permute-done.47.refs_1_ = bf16[256,4096]{1,0:T(8,128)(2,1)} collective-permute-done((bf16[256,4096]{1,0:T(8,128)(2,1)}, bf16[256,4096]{1,0:T(8,128)(2,1)}, u32[]{:S(2)}, u32[]{:S(2)}) %collective-permute-start.47) | collective-permute-done | bytes 2097184 | tf_op jit(solution)/shard_map/ppermute | solution.py:712
  1116.7 44.4 %collective-permute-done.41.refs_3_ = bf16[256,4096]{1,0:T(8,128)(2,1)} collective-permute-done((bf16[256,4096]{1,0:T(8,128)(2,1)}, bf16[256,4096]{1,0:T(8,128)(2,1)}, u32[]{:S(2)}, u32[]{:S(2)}) %collective-permute-start.41) | collective-permute-done | bytes 2097184 | tf_op jit(solution)/shard_map/ppermute | solution.py:712
  1161.1 5.8 zsum.6.refs_0_
  1166.9 4.4 add_convert_fusion.refs_7_
  1173.0 48.0 %mlp.8 = (bf16[256,4096]{1,0:T(8,128)(2,1)}, bf16[256,4096]{1,0:T(8,128)(2,1)}) custom-call(bf16[256,4096]{1,0:T(8,128)(2,1)} %get-tuple-element.137.refs_0_, bf16[256,4096]{1,0:T(8,128)(2,1)} %collective-permute-done.47.refs_1_, bf16[256,4096]{1,0:T(8,128)(2,1)} %collective-permute-done.48.refs_2_, bf16[256,4096]{1,0:T(8,128)(2,1)} %collective-permute-done.49.refs_3_, ...), custom_call_target="tpu_custom_call" | custom-call | flops 38654705664 | bytes 75497472 | tf_op jit(solution)/shard_map/mlp/pallas_call | solution.py:577
  1221.0 5.6 zsum.7.refs_0_
  1229.4 48.0 %mlp.9 = (bf16[256,4096]{1,0:T(8,128)(2,1)}, bf16[256,4096]{1,0:T(8,128)(2,1)}) custom-call(bf16[256,4096]{1,0:T(8,128)(2,1)} %get-tuple-element.137.refs_0_, bf16[256,4096]{1,0:T(8,128)(2,1)} %collective-permute-done.47.refs_1_, bf16[256,4096]{1,0:T(8,128)(2,1)} %collective-permute-done.48.refs_2_, bf16[256,4096]{1,0:T(8,128)(2,1)} %collective-permute-done.49.refs_3_, ...), custom_call_target="tpu_custom_call" | custom-call | flops 38654705664 | bytes 75497472 | tf_op jit(solution)/shard_map/mlp/pallas_call | solution.py:577
  1278.2 3.7 collective-permute-done.52.refs_2_
  1286.0 18.2 %collective-permute-done.51.refs_3_ = bf16[128,4096]{1,0:T(8,128)(2,1)} collective-permute-done((bf16[128,4096]{1,0:T(8,128)(2,1)}, bf16[128,4096]{1,0:T(8,128)(2,1)}, u32[]{:S(2)}, u32[]{:S(2)}) %collective-permute-start.51) | collective-permute-done | bytes 1048608 | tf_op jit(solution)/shard_map/ppermute | solution.py:712
  1307.4 18.3 %collective-permute-done.53.refs_3_ = bf16[128,4096]{1,0:T(8,128)(2,1)} collective-permute-done((bf16[128,4096]{1,0:T(8,128)(2,1)}, bf16[128,4096]{1,0:T(8,128)(2,1)}, u32[]{:S(2)}, u32[]{:S(2)}) %collective-permute-start.53) | collective-permute-done | bytes 1048608 | tf_op jit(solution)/shard_map/ppermute | solution.py:712
  (108 shorter events, 86.2 us)
Async XLA Ops:
  4.7 73.1 %collective-permute-start.6 = (bf16[256,4096]{1,0:T(8,128)(2,1)}, bf16[256,4096]{1,0:T(8,128)(2,1)}, u32[]{:S(2)}, u32[]{:S(2)}) collective-permute-start(bf16[256,4096]{1,0:T(8,128)(2,1)} %norm.4.refs_2_.refs_0_), channel_id=1, source_target_pairs={{0,2},{1,3},{2,0},{3,1},{4,6},{5,7},{6,4},{7,5}} | collective-permute-start | bytes 6291464 | tf_op jit(solution)/shard_map/ppermute | solution.py:712
  8.0 30.1 %collective-permute-start = (bf16[256,4096]{1,0:T(8,128)(2,1)}, bf16[256,4096]{1,0:T(8,128)(2,1)}, u32[]{:S(2)}, u32[]{:S(2)}) collective-permute-start(bf16[256,4096]{1,0:T(8,128)(2,1)} %norm.4.refs_2_.refs_0_), channel_id=1, source_target_pairs={{0,1},{1,0},{2,3},{3,2},{4,5},{5,4},{6,7},{7,6}} | collective-permute-start | bytes 6291464 | tf_op jit(solution)/shard_map/ppermute | solution.py:712
  11.5 26.7 %collective-permute-start.1 = (bf16[256,4096]{1,0:T(8,128)(2,1)}, bf16[256,4096]{1,0:T(8,128)(2,1)}, u32[]{:S(2)}, u32[]{:S(2)}) collective-permute-start(bf16[256,4096]{1,0:T(8,128)(2,1)} %norm.5.refs_2_.refs_1_), channel_id=1, source_target_pairs={{0,1},{1,0},{2,3},{3,2},{4,5},{5,4},{6,7},{7,6}} | collective-permute-start | bytes 6291464 | tf_op jit(solution)/shard_map/ppermute | solution.py:712
  15.4 22.7 %collective-permute-start.2 = (bf16[256,4096]{1,0:T(8,128)(2,1)}, bf16[256,4096]{1,0:T(8,128)(2,1)}, u32[]{:S(2)}, u32[]{:S(2)}) collective-permute-start(bf16[256,4096]{1,0:T(8,128)(2,1)} %norm.6.refs_2_), channel_id=1, source_target_pairs={{0,1},{1,0},{2,3},{3,2},{4,5},{5,4},{6,7},{7,6}} | collective-permute-start | bytes 6291464 | tf_op jit(solution)/shard_map/ppermute | solution.py:712
  18.9 19.3 %collective-permute-start.3 = (bf16[256,4096]{1,0:T(8,128)(2,1)}, bf16[256,4096]{1,0:T(8,128)(2,1)}, u32[]{:S(2)}, u32[]{:S(2)}) collective-permute-start(bf16[256,4096]{1,0:T(8,128)(2,1)} %norm.7.refs_3_), channel_id=1, source_target_pairs={{0,1},{1,0},{2,3},{3,2},{4,5},{5,4},{6,7},{7,6}} | collective-permute-start | bytes 6291464 | tf_op jit(solution)/shard_map/ppermute | solution.py:712
  77.9 48.3 %collective-permute-start.8 = (bf16[256,4096]{1,0:T(8,128)(2,1)}, bf16[256,4096]{1,0:T(8,128)(2,1)}, u32[]{:S(2)}, u32[]{:S(2)}) collective-permute-start(bf16[256,4096]{1,0:T(8,128)(2,1)} %norm.5.refs_2_.refs_1_), channel_id=1, source_target_pairs={{0,2},{1,3},{2,0},{3,1},{4,6},{5,7},{6,4},{7,5}} | collective-permute-start | bytes 6291464 | tf_op jit(solution)/shard_map/ppermute | solution.py:712
  126.2 83.4 %collective-permute-start.5 = (bf16[256,4096]{1,0:T(8,128)(2,1)}, bf16[256,4096]{1,0:T(8,128)(2,1)}, u32[]{:S(2)}, u32[]{:S(2)}) collective-permute-start(bf16[256,4096]{1,0:T(8,128)(2,1)} %norm.6.refs_2_), channel_id=1, source_target_pairs={{0,2},{1,3},{2,0},{3,1},{4,6},{5,7},{6,4},{7,5}} | collective-permute-start | bytes 6291464 | tf_op jit(solution)/shard_map/ppermute | solution.py:712
  209.6 5.8 collective-permute-start.10
  211.3 47.9 %collective-permute-start.4 = (bf16[256,4096]{1,0:T(8,128)(2,1)}, bf16[256,4096]{1,0:T(8,128)(2,1)}, u32[]{:S(2)}, u32[]{:S(2)}) collective-permute-start(bf16[256,4096]{1,0:T(8,128)(2,1)} %norm.7.refs_3_), channel_id=1, source_target_pairs={{0,2},{1,3},{2,0},{3,1},{4,6},{5,7},{6,4},{7,5}} | collective-permute-start | bytes 6291464 | tf_op jit(solution)/shard_map/ppermute | solution.py:712
  259.2 48.8 %collective-permute-start.12 = (bf16[8,2,256,256]{3,2,1,0:T(8,128)(2,1)}, bf16[8,2,256,256]{3,2,1,0:T(8,128)(2,1)}, u32[]{:S(2)}, u32[]{:S(2)}) collective-permute-start(bf16[8,2,256,256]{3,2,1,0:T(8,128)(2,1)} %get-tuple-element.80.refs_5_.refs_4_.refs_3_), channel_id=1, source_target_pairs={{0,4},{4,0},{1,5},{5,1},{2,6},{6,2},{3,7},{7,3}} | collective-permute-start | bytes 6291464 | tf_op jit(solution)/shard_map/ppermute | solution.py:712
  262.1 57.1 %collective-permute-start.13 = (bf16[2,2,256,256]{3,2,1,0:T(8,128)(2,1)}, bf16[2,2,256,256]{3,2,1,0:T(8,128)(2,1)}, u32[]{:S(2)}, u32[]{:S(2)}) collective-permute-start(bf16[2,2,256,256]{3,2,1,0:T(8,128)(2,1)} %get-tuple-element.83.refs_5_.refs_4_), channel_id=1, source_target_pairs={{0,4},{4,0},{1,5},{5,1},{2,6},{6,2},{3,7},{7,3}} | collective-permute-start | bytes 1572872 | tf_op jit(solution)/shard_map/ppermute | solution.py:712
  262.5 68.0 %collective-permute-start.14 = (bf16[2,2,256,256]{3,2,1,0:T(8,128)(2,1)}, bf16[2,2,256,256]{3,2,1,0:T(8,128)(2,1)}, u32[]{:S(2)}, u32[]{:S(2)}) collective-permute-start(bf16[2,2,256,256]{3,2,1,0:T(8,128)(2,1)} %get-tuple-element.86.refs_6_.refs_5_), channel_id=1, source_target_pairs={{0,4},{4,0},{1,5},{5,1},{2,6},{6,2},{3,7},{7,3}} | collective-permute-start | bytes 1572872 | tf_op jit(solution)/shard_map/ppermute | solution.py:712
  264.1 77.6 %collective-permute-start.15 = (bf16[2,2,256,256]{3,2,1,0:T(8,128)(2,1)}, bf16[2,2,256,256]{3,2,1,0:T(8,128)(2,1)}, u32[]{:S(2)}, u32[]{:S(2)}) collective-permute-start(bf16[2,2,256,256]{3,2,1,0:T(8,128)(2,1)} %get-tuple-element.89.refs_5_.refs_6_), channel_id=1, source_target_pairs={{0,4},{4,0},{1,5},{5,1},{2,6},{6,2},{3,7},{7,3}} | collective-permute-start | bytes 1572872 | tf_op jit(solution)/shard_map/ppermute | solution.py:712
  272.4 80.1 %collective-permute-start.16 = (bf16[2,2,256,256]{3,2,1,0:T(8,128)(2,1)}, bf16[2,2,256,256]{3,2,1,0:T(8,128)(2,1)}, u32[]{:S(2)}, u32[]{:S(2)}) collective-permute-start(bf16[2,2,256,256]{3,2,1,0:T(8,128)(2,1)} %qkv.10.refs_5_.refs_7_), channel_id=1, source_target_pairs={{0,4},{4,0},{1,5},{5,1},{2,6},{6,2},{3,7},{7,3}} | collective-permute-start | bytes 1572872 | tf_op jit(solution)/shard_map/ppermute | solution.py:712
  308.0 176.5 %collective-permute-start.20 = (bf16[1024,4096]{1,0:T(8,128)(2,1)}, bf16[1024,4096]{1,0:T(8,128)(2,1)}, u32[]{:S(2)}, u32[]{:S(2)}) collective-permute-start(bf16[1024,4096]{1,0:T(8,128)(2,1)} %bitcast.24), channel_id=1, source_target_pairs={{0,1},{1,0},{2,3},{3,2},{4,5},{5,4},{6,7},{7,6}} | collective-permute-start | bytes 25165832 | tf_op jit(solution)/shard_map/ppermute | solution.py:712
  319.2 62.4 %collective-permute-start.21 = (bf16[256,4096]{1,0:T(8,128)(2,1)}, bf16[256,4096]{1,0:T(8,128)(2,1)}, u32[]{:S(2)}, u32[]{:S(2)}) collective-permute-start(bf16[256,4096]{1,0:T(8,128)(2,1)} %get-tuple-element.101), channel_id=1, source_target_pairs={{0,2},{1,3},{2,0},{3,1},{4,6},{5,7},{6,4},{7,5}} | collective-permute-start | bytes 6291464 | tf_op jit(solution)/shard_map/ppermute | solution.py:712
  330.5 96.4 %collective-permute-start.22 = (bf16[256,4096]{1,0:T(8,128)(2,1)}, bf16[256,4096]{1,0:T(8,128)(2,1)}, u32[]{:S(2)}, u32[]{:S(2)}) collective-permute-start(bf16[256,4096]{1,0:T(8,128)(2,1)} %get-tuple-element.103), channel_id=1, source_target_pairs={{0,2},{1,3},{2,0},{3,1},{4,6},{5,7},{6,4},{7,5}} | collective-permute-start | bytes 6291464 | tf_op jit(solution)/shard_map/ppermute | solution.py:712
  381.6 47.5 %collective-permute-start.23 = (bf16[256,4096]{1,0:T(8,128)(2,1)}, bf16[256,4096]{1,0:T(8,128)(2,1)}, u32[]{:S(2)}, u32[]{:S(2)}) collective-permute-start(bf16[256,4096]{1,0:T(8,128)(2,1)} %collective-permute-done.21.refs_6_), channel_id=1, source_target_pairs={{0,4},{4,0},{1,5},{5,1},{2,6},{6,2},{3,7},{7,3}} | collective-permute-start | bytes 6291464 | tf_op jit(solution)/shard_map/ppermute | solution.py:712
  426.9 50.1 %collective-permute-start.17 = (bf16[2,256,1024]{2,1,0:T(8,128)(2,1)}, bf16[2,256,1024]{2,1,0:T(8,128)(2,1)}, u32[]{:S(2)}, u32[]{:S(2)}) collective-permute-start(bf16[2,256,1024]{2,1,0:T(8,128)(2,1)} %get-tuple-element.97), channel_id=1, source_target_pairs={{0,1},{1,0},{2,3},{3,2},{4,5},{5,4},{6,7},{7,6}} | collective-permute-start | bytes 3145736 | tf_op jit(solution)/shard_map/ppermute | solution.py:712
  426.9 50.5 %collective-permute-start.18 = (bf16[2,256,1024]{2,1,0:T(8,128)(2,1)}, bf16[2,256,1024]{2,1,0:T(8,128)(2,1)}, u32[]{:S(2)}, u32[]{:S(2)}) collective-permute-start(bf16[2,256,1024]{2,1,0:T(8,128)(2,1)} %get-tuple-element.98), channel_id=1, source_target_pairs={{0,2},{1,3},{2,0},{3,1},{4,6},{5,7},{6,4},{7,5}} | collective-permute-start | bytes 3145736 | tf_op jit(solution)/shard_map/ppermute | solution.py:712
  427.9 49.6 %collective-permute-start.19 = (bf16[2,256,1024]{2,1,0:T(8,128)(2,1)}, bf16[2,256,1024]{2,1,0:T(8,128)(2,1)}, u32[]{:S(2)}, u32[]{:S(2)}) collective-permute-start(bf16[2,256,1024]{2,1,0:T(8,128)(2,1)} %get-tuple-element.99), channel_id=1, source_target_pairs={{0,3},{1,2},{2,1},{3,0},{4,7},{5,6},{6,5},{7,4}} | collective-permute-start | bytes 3145736 | tf_op jit(solution)/shard_map/ppermute | solution.py:712
  429.1 47.8 %collective-permute-start.24 = (bf16[256,4096]{1,0:T(8,128)(2,1)}, bf16[256,4096]{1,0:T(8,128)(2,1)}, u32[]{:S(2)}, u32[]{:S(2)}) collective-permute-start(bf16[256,4096]{1,0:T(8,128)(2,1)} %collective-permute-done.22.refs_7_), channel_id=1, source_target_pairs={{0,4},{4,0},{1,5},{5,1},{2,6},{6,2},{3,7},{7,3}} | collective-permute-start | bytes 6291464 | tf_op jit(solution)/shard_map/ppermute | solution.py:712
  476.9 7.5 collective-permute-start.26
  477.5 10.0 collective-permute-start.27
  477.5 13.0 collective-permute-start.28
  519.5 53.9 %collective-permute-start.30 = (bf16[256,4096]{1,0:T(8,128)(2,1)}, bf16[256,4096]{1,0:T(8,128)(2,1)}, u32[]{:S(2)}, u32[]{:S(2)}) collective-permute-start(bf16[256,4096]{1,0:T(8,128)(2,1)} %get-tuple-element.109.refs_0_), channel_id=1, source_target_pairs={{0,1},{1,0},{2,3},{3,2},{4,5},{5,4},{6,7},{7,6}} | collective-permute-start | bytes 6291464 | tf_op jit(solution)/shard_map/ppermute | solution.py:712
  519.7 53.8 %collective-permute-start.29 = (bf16[256,4096]{1,0:T(8,128)(2,1)}, bf16[256,4096]{1,0:T(8,128)(2,1)}, u32[]{:S(2)}, u32[]{:S(2)}) collective-permute-start(bf16[256,4096]{1,0:T(8,128)(2,1)} %get-tuple-element.109.refs_0_), channel_id=1, source_target_pairs={{0,2},{1,3},{2,0},{3,1},{4,6},{5,7},{6,4},{7,5}} | collective-permute-start | bytes 6291464 | tf_op jit(solution)/shard_map/ppermute | solution.py:712
  664.6 121.8 %collective-permute-start.32 = (bf16[512,4096]{1,0:T(8,128)(2,1)}, bf16[512,4096]{1,0:T(8,128)(2,1)}, u32[]{:S(2)}, u32[]{:S(2)}) collective-permute-start(bf16[512,4096]{1,0:T(8,128)(2,1)} %get-tuple-element.119), channel_id=1, source_target_pairs={{0,1},{1,0},{2,3},{3,2},{4,5},{5,4},{6,7},{7,6}} | collective-permute-start | bytes 12582920 | tf_op jit(solution)/shard_map/ppermute | solution.py:712
  664.8 48.8 %collective-permute-start.37 = (bf16[256,4096]{1,0:T(8,128)(2,1)}, bf16[256,4096]{1,0:T(8,128)(2,1)}, u32[]{:S(2)}, u32[]{:S(2)}) collective-permute-start(bf16[256,4096]{1,0:T(8,128)(2,1)} %get-tuple-element.126.refs_0_), channel_id=1, source_target_pairs={{0,2},{1,3},{2,0},{3,1},{4,6},{5,7},{6,4},{7,5}} | collective-permute-start | bytes 6291464 | tf_op jit(solution)/shard_map/ppermute | solution.py:712
  666.5 47.1 %collective-permute-start.33 = (bf16[2,256,1024]{2,1,0:T(8,128)(2,1)}, bf16[2,256,1024]{2,1,0:T(8,128)(2,1)}, u32[]{:S(2)}, u32[]{:S(2)}) collective-permute-start(bf16[2,256,1024]{2,1,0:T(8,128)(2,1)} %get-tuple-element.121), channel_id=1, source_target_pairs={{0,1},{1,0},{2,3},{3,2},{4,5},{5,4},{6,7},{7,6}} | collective-permute-start | bytes 3145736 | tf_op jit(solution)/shard_map/ppermute | solution.py:712
  666.6 69.5 %collective-permute-start.34 = (bf16[2,256,1024]{2,1,0:T(8,128)(2,1)}, bf16[2,256,1024]{2,1,0:T(8,128)(2,1)}, u32[]{:S(2)}, u32[]{:S(2)}) collective-permute-start(bf16[2,256,1024]{2,1,0:T(8,128)(2,1)} %get-tuple-element.122), channel_id=1, source_target_pairs={{0,2},{1,3},{2,0},{3,1},{4,6},{5,7},{6,4},{7,5}} | collective-permute-start | bytes 3145736 | tf_op jit(solution)/shard_map/ppermute | solution.py:712
  666.9 90.4 %collective-permute-start.35 = (bf16[2,256,1024]{2,1,0:T(8,128)(2,1)}, bf16[2,256,1024]{2,1,0:T(8,128)(2,1)}, u32[]{:S(2)}, u32[]{:S(2)}) collective-permute-start(bf16[2,256,1024]{2,1,0:T(8,128)(2,1)} %get-tuple-element.123), channel_id=1, source_target_pairs={{0,3},{1,2},{2,1},{3,0},{4,7},{5,6},{6,5},{7,4}} | collective-permute-start | bytes 3145736 | tf_op jit(solution)/shard_map/ppermute | solution.py:712
  713.6 77.1 %collective-permute-start.38 = (bf16[256,4096]{1,0:T(8,128)(2,1)}, bf16[256,4096]{1,0:T(8,128)(2,1)}, u32[]{:S(2)}, u32[]{:S(2)}) collective-permute-start(bf16[256,4096]{1,0:T(8,128)(2,1)} %get-tuple-element.126.refs_0_), channel_id=1, source_target_pairs={{0,1},{1,0},{2,3},{3,2},{4,5},{5,4},{6,7},{7,6}} | collective-permute-start | bytes 6291464 | tf_op jit(solution)/shard_map/ppermute | solution.py:712
  713.6 77.1 %collective-permute-start.39 = (bf16[256,4096]{1,0:T(8,128)(2,1)}, bf16[256,4096]{1,0:T(8,128)(2,1)}, u32[]{:S(2)}, u32[]{:S(2)}) collective-permute-start(bf16[256,4096]{1,0:T(8,128)(2,1)} %collective-permute-done.37.refs_1_), channel_id=1, source_target_pairs={{0,1},{1,0},{2,3},{3,2},{4,5},{5,4},{6,7},{7,6}} | collective-permute-start | bytes 6291464 | tf_op jit(solution)/shard_map/ppermute | solution.py:712
  877.7 98.9 %collective-permute-start.40 = (bf16[512,4096]{1,0:T(8,128)(2,1)}, bf16[512,4096]{1,0:T(8,128)(2,1)}, u32[]{:S(2)}, u32[]{:S(2)}) collective-permute-start(bf16[512,4096]{1,0:T(8,128)(2,1)} %get-tuple-element.129), channel_id=1, source_target_pairs={{0,1},{1,0},{2,3},{3,2},{4,5},{5,4},{6,7},{7,6}} | collective-permute-start | bytes 12582920 | tf_op jit(solution)/shard_map/ppermute | solution.py:712
  878.2 48.8 %collective-permute-start.42 = (bf16[256,4096]{1,0:T(8,128)(2,1)}, bf16[256,4096]{1,0:T(8,128)(2,1)}, u32[]{:S(2)}, u32[]{:S(2)}) collective-permute-start(bf16[256,4096]{1,0:T(8,128)(2,1)} %get-tuple-element.132.refs_0_), channel_id=1, source_target_pairs={{0,2},{1,3},{2,0},{3,1},{4,6},{5,7},{6,4},{7,5}} | collective-permute-start | bytes 6291464 | tf_op jit(solution)/shard_map/ppermute | solution.py:712
  879.9 91.2 %collective-permute-start.36 = (bf16[256,4096]{1,0:T(8,128)(2,1)}, bf16[256,4096]{1,0:T(8,128)(2,1)}, u32[]{:S(2)}, u32[]{:S(2)}) collective-permute-start(bf16[256,4096]{1,0:T(8,128)(2,1)} %add_convert_fusion.2.refs_7_), channel_id=1, source_target_pairs={{0,2},{1,3},{2,0},{3,1},{4,6},{5,7},{6,4},{7,5}} | collective-permute-start | bytes 6291464 | tf_op jit(solution)/shard_map/ppermute | solution.py:712
  880.2 100.8 %collective-permute-start.43 = (bf16[256,4096]{1,0:T(8,128)(2,1)}, bf16[256,4096]{1,0:T(8,128)(2,1)}, u32[]{:S(2)}, u32[]{:S(2)}) collective-permute-start(bf16[256,4096]{1,0:T(8,128)(2,1)} %get-tuple-element.132.refs_0_), channel_id=1, source_target_pairs={{0,1},{1,0},{2,3},{3,2},{4,5},{5,4},{6,7},{7,6}} | collective-permute-start | bytes 6291464 | tf_op jit(solution)/shard_map/ppermute | solution.py:712
  927.0 54.0 %collective-permute-start.44 = (bf16[256,4096]{1,0:T(8,128)(2,1)}, bf16[256,4096]{1,0:T(8,128)(2,1)}, u32[]{:S(2)}, u32[]{:S(2)}) collective-permute-start(bf16[256,4096]{1,0:T(8,128)(2,1)} %collective-permute-done.42.refs_1_), channel_id=1, source_target_pairs={{0,1},{1,0},{2,3},{3,2},{4,5},{5,4},{6,7},{7,6}} | collective-permute-start | bytes 6291464 | tf_op jit(solution)/shard_map/ppermute | solution.py:712
  1067.8 99.1 %collective-permute-start.45 = (bf16[512,4096]{1,0:T(8,128)(2,1)}, bf16[512,4096]{1,0:T(8,128)(2,1)}, u32[]{:S(2)}, u32[]{:S(2)}) collective-permute-start(bf16[512,4096]{1,0:T(8,128)(2,1)} %get-tuple-element.135), channel_id=1, source_target_pairs={{0,1},{1,0},{2,3},{3,2},{4,5},{5,4},{6,7},{7,6}} | collective-permute-start | bytes 12582920 | tf_op jit(solution)/shard_map/ppermute | solution.py:712
  1067.8 48.8 %collective-permute-start.47 = (bf16[256,4096]{1,0:T(8,128)(2,1)}, bf16[256,4096]{1,0:T(8,128)(2,1)}, u32[]{:S(2)}, u32[]{:S(2)}) collective-permute-start(bf16[256,4096]{1,0:T(8,128)(2,1)} %get-tuple-element.137.refs_0_), channel_id=1, source_target_pairs={{0,2},{1,3},{2,0},{3,1},{4,6},{5,7},{6,4},{7,5}} | collective-permute-start | bytes 6291464 | tf_op jit(solution)/shard_map/ppermute | solution.py:712
  1069.5 91.5 %collective-permute-start.41 = (bf16[256,4096]{1,0:T(8,128)(2,1)}, bf16[256,4096]{1,0:T(8,128)(2,1)}, u32[]{:S(2)}, u32[]{:S(2)}) collective-permute-start(bf16[256,4096]{1,0:T(8,128)(2,1)} %add_convert_fusion.1.refs_7_), channel_id=1, source_target_pairs={{0,2},{1,3},{2,0},{3,1},{4,6},{5,7},{6,4},{7,5}} | collective-permute-start | bytes 6291464 | tf_op jit(solution)/shard_map/ppermute | solution.py:712
  1069.9 103.2 %collective-permute-start.48 = (bf16[256,4096]{1,0:T(8,128)(2,1)}, bf16[256,4096]{1,0:T(8,128)(2,1)}, u32[]{:S(2)}, u32[]{:S(2)}) collective-permute-start(bf16[256,4096]{1,0:T(8,128)(2,1)} %get-tuple-element.137.refs_0_), channel_id=1, source_target_pairs={{0,1},{1,0},{2,3},{3,2},{4,5},{5,4},{6,7},{7,6}} | collective-permute-start | bytes 6291464 | tf_op jit(solution)/shard_map/ppermute | solution.py:712
  1116.6 56.4 %collective-permute-start.49 = (bf16[256,4096]{1,0:T(8,128)(2,1)}, bf16[256,4096]{1,0:T(8,128)(2,1)}, u32[]{:S(2)}, u32[]{:S(2)}) collective-permute-start(bf16[256,4096]{1,0:T(8,128)(2,1)} %collective-permute-done.47.refs_1_), channel_id=1, source_target_pairs={{0,1},{1,0},{2,3},{3,2},{4,5},{5,4},{6,7},{7,6}} | collective-permute-start | bytes 6291464 | tf_op jit(solution)/shard_map/ppermute | solution.py:712
  1171.3 49.7 %collective-permute-start.46 = (bf16[256,4096]{1,0:T(8,128)(2,1)}, bf16[256,4096]{1,0:T(8,128)(2,1)}, u32[]{:S(2)}, u32[]{:S(2)}) collective-permute-start(bf16[256,4096]{1,0:T(8,128)(2,1)} %add_convert_fusion.refs_7_), channel_id=1, source_target_pairs={{0,2},{1,3},{2,0},{3,1},{4,6},{5,7},{6,4},{7,5}} | collective-permute-start | bytes 6291464 | tf_op jit(solution)/shard_map/ppermute | solution.py:712
  1221.0 5.6 collective-permute-start.50
  1277.8 26.3 %collective-permute-start.51 = (bf16[128,4096]{1,0:T(8,128)(2,1)}, bf16[128,4096]{1,0:T(8,128)(2,1)}, u32[]{:S(2)}, u32[]{:S(2)}) collective-permute-start(bf16[128,4096]{1,0:T(8,128)(2,1)} %add_convert_fusion.4.refs_7_), channel_id=1, source_target_pairs={{0,2},{1,3},{2,0},{3,1},{4,6},{5,7},{6,4},{7,5}} | collective-permute-start | bytes 3145736 | tf_op jit(solution)/shard_map/ppermute | solution.py:712
  1285.6 40.1 %collective-permute-start.53 = (bf16[128,4096]{1,0:T(8,128)(2,1)}, bf16[128,4096]{1,0:T(8,128)(2,1)}, u32[]{:S(2)}, u32[]{:S(2)}) collective-permute-start(bf16[128,4096]{1,0:T(8,128)(2,1)} %add_convert_fusion.3.refs_5_), channel_id=1, source_target_pairs={{0,2},{1,3},{2,0},{3,1},{4,6},{5,7},{6,4},{7,5}} | collective-permute-start | bytes 3145736 | tf_op jit(solution)/shard_map/ppermute | solution.py:712
  (9 other events, 35.9 us)

commit v11 on v9

--- a/solution.py
+++ b/solution.py
@@ -15,14 +15,12 @@
 NEG = -1e30
 LOG2E = math.log2(math.e)
 DN = (((1,), (0,)), ((), ()))
-VMEM = 67043328
 BF = jnp.bfloat16
 F32 = jnp.float32
 ANY = pl.BlockSpec(memory_space=pltpu.HBM)
 
 
-def params(n):
-    return pltpu.CompilerParams(dimension_semantics=("arbitrary",) * n, vmem_limit_bytes=VMEM)
+PARAMS = pltpu.CompilerParams(vmem_limit_bytes=67043328)
 
 
 def rope_tables(positions):
@@ -60,7 +58,7 @@
         + [ANY] * len(after),
         out_specs=pl.BlockSpec((tile, dim), lambda i: (i, 0)),
         out_shape=jax.ShapeDtypeStruct((RUN, dim), BF),
-        name="norm", compiler_params=params(1),
+        name="norm", compiler_params=PARAMS,
         cost_estimate=cost(RUN * dim, RUN * dim),
     )(x_rows, gain, *after)
 
@@ -89,25 +87,28 @@
                 rows = pl.ds(pl.multiple_of((k * group + i) * RUN, RUN), RUN)
                 pltpu.make_async_copy(a_scr.at[rows, :], a_scr.at[rows, :], sem.at[k * group + i]).wait()
 
-        rows = pl.ds(pl.multiple_of(k * group * RUN, group * RUN), group * RUN)
-        r = jnp.dot(a_scr[rows, :], w_ref[...], preferred_element_type=F32)
-
-        def piece(i, h):
-            return r[i * RUN:(i + 1) * RUN, h * HD:(h + 1) * HD].T
-
-        @pl.when((n < n_q) if with_q else False)
-        def _():
-            for i in range(group):
-                for h in range(heads):
-                    q_ref[k * group + i, h * HD:(h + 1) * HD, :] = rope(piece(i, h), k * group + i).astype(BF)
-
-        @pl.when((n == n_q) if with_kv else False)
-        def _():
-            for i in range(group):
-                for h in range(heads // 2):
-                    kv_ref[k * group + i, 0, :, h * HD:(h + 1) * HD] = rope(piece(i, h), k * group + i).T.astype(BF)
-                    kv_ref[k * group + i, 1, h * HD:(h + 1) * HD, :] = piece(i, h + heads // 2).astype(BF)
-
+        runs = [k * group + i for i in range(group)]
+
+        def products():
+            return [jnp.dot(a_scr[pl.ds(pl.multiple_of(run * RUN, RUN), RUN), :], w_ref[...], preferred_element_type=F32)
+                    for run in runs]
+
+        if with_q:
+            @pl.when(n < n_q)
+            def _():
+                for run, r in zip(runs, products()):
+                    for h in range(heads):
+                        cols = slice(h * HD, (h + 1) * HD)
+                        q_ref[run, cols, :] = rope(r[:, cols].T, run).astype(BF)
+
+        if with_kv:
+            @pl.when(n == n_q)
+            def _():
+                for run, r in zip(runs, products()):
+                    for h in range(heads // 2):
+                        cols, past = slice(h * HD, (h + 1) * HD), heads // 2 * HD
+                        kv_ref[run, 0, :, cols] = rope(r[:, cols].T, run).T.astype(BF)
+                        kv_ref[run, 1, cols, :] = r[:, past + h * HD:past + (h + 1) * HD].T.astype(BF)
         return carry
 
     lax.fori_loop(0, n_in // group, one, 0)
@@ -132,7 +133,7 @@
         + [pl.BlockSpec(kv_shape, lambda n: (0,) * len(kv_shape))] * with_kv,
         out_shape=[jax.ShapeDtypeStruct((n_in, n_q * tn, RUN), BF)] * with_q + [jax.ShapeDtypeStruct(kv_shape, BF)] * with_kv,
         scratch_shapes=[pltpu.VMEM((n_in * RUN, dim), BF), pltpu.SemaphoreType.DMA((n_in,))],
-        name="qkv", compiler_params=params(1),
+        name="qkv", compiler_params=PARAMS,
         cost_estimate=cost(2 * n_in * RUN * w_all.size, 2 * w_all.size),
     )(*rows, w_all, cos, sin, *after)
 
@@ -403,7 +404,7 @@
                             pltpu.SemaphoreType.DMA((n_tiles,)), *scratch]),
         out_shape=out_shape,
         input_output_aliases={n_in - len(old) + k: k for k in range(len(old))},
-        name="flash" if final else "flash_part", compiler_params=params(0),
+        name="flash" if final else "flash_part", compiler_params=PARAMS,
         cost_estimate=cost(8 * work * RUN * RUN * nq, n_runs * RUN * nq),
     )(tab, *qs, *kvs, *sts, *more, *after)
 
@@ -498,7 +499,7 @@
         scratch_shapes=[pltpu.VMEM((rows, 4 * width), BF), pltpu.VMEM((3, width // 2, dim), BF), pltpu.VMEM((rows, dim), BF),
                         pltpu.VMEM((rows, dim), F32), pltpu.SemaphoreType.DMA((len(blocks), 2 * n_run)),
                         pltpu.SemaphoreType.DMA((3,)), pltpu.SemaphoreType.DMA, pltpu.SemaphoreType.DMA((2 * n_run,))],
-        name="outp", compiler_params=params(1),
+        name="outp", compiler_params=PARAMS,
         cost_estimate=cost(8 * rows * width * dim, 8 * width * dim),
     )(*os, *ws, x_rows, gain, *after)
 
@@ -582,7 +583,7 @@
         scratch_shapes=[pltpu.VMEM((rows, dim), BF), pltpu.VMEM((rows, ffn), BF), pltpu.VMEM((2, 2, dim, tn), BF),
                         pltpu.VMEM((2, ffn, td), BF), pltpu.SemaphoreType.DMA((len(bs),)), pltpu.SemaphoreType.DMA((2,)),
                         pltpu.SemaphoreType.DMA((2,))],
-        name="mlp", compiler_params=params(1),
+        name="mlp", compiler_params=PARAMS,
         cost_estimate=cost(6 * rows * dim * ffn, 6 * dim * ffn),
     )(*bs, wg, wu, wd, *after)
 
@@ -603,7 +604,7 @@
         out_specs=at(first),
         out_shape=jax.ShapeDtypeStruct((total, dim), BF),
         input_output_aliases={0: 0} if prev else {},
-        name="zsum", compiler_params=params(1),
+        name="zsum", compiler_params=PARAMS,
         cost_estimate=cost(rows * dim, 8 * rows * dim),
     )(*prev, keep, recv, far, y, *after)
 
@@ -650,8 +651,9 @@
 
 def work_tables(cps, piece):
     per = piece // 2 // RUN
-    early = 2 * per + 2
+    early, more = 2 * per + 2, 2 * per + 4
     stage = lambda r: 0 if r < early else 1
+    soon_pair = lambda r, t: r < early and t < early or r < more and t in (0, 1, per, per + 1)
     calls = [(0, list(range(early)))]
     calls += [(1, [j, per + j, 2 * per + 2 * j, 2 * per + 2 * j + 1]) for j in range(per)]
     tabs, all_runs, sizes = [], [], []
@@ -667,7 +669,7 @@
                     pairs, carry = [], []
                     for t in tiles:
                         seen = [r for r in range(len(pos)) if pos[r] < pos[t]]
-                        when = {r: max(stage(r), stage(t)) for r in seen}
+                        when = {r: 0 if soon_pair(r, t) else 1 for r in seen}
                         late = list(when.values()).count(1) + stage(t)
                         soon = len(seen) + 1 - late
                         if late and soon % 4 <= -late % 4:
@@ -744,8 +746,8 @@
         wo_c = send(over_core, tied(wo, kvs[-1]))
 
         tiles = [(0, i) for i in range(2 * n_run)] + [(1, 0), (1, 1)]
-        st, *wo_x = flash(tab, [q_here, q_far[0]], tiles, kvs[:2], base=bases[0], work=int(work[0]), cut=wo,
-                         n_cut=n_piece, after=(kvs[-1],))
+        st, *wo_x = flash(tab, [q_here, q_far[0]], tiles, kvs, base=bases[0], work=int(work[0]), cut=wo,
+                         n_cut=n_piece)
         wo_x = [send(over_x, w) for w in wo_x]
         far_qkv(3, far_qkv(2, st))
         kvs = kvs + [send(over_y, kv) for kv in kvs]

time: 1330 us -> 1320 us (level)
  transfers between devices with their start and end apart: 54 -> 54, of which waited for: 27 -> 28; matrix products, arithmetic and copies ran while one was open for 3% -> 3% of each run, Pallas kernels for 32% -> 32%
where the time goes in v11:
time: 1320 us; the launch traced here: 1310 us
  Pallas kernels  760 us (58%)
  waiting for transfers between devices  468 us (35%)
  starting transfers between devices  40 us (3%)
  other arithmetic  23.2 us (2%)
  local copies, waits for them, and re-layouts  19.2 us (1%)
    ppermute x54, waiting for transfers between devices, send(): return lax.ppermute(v, *axis_pairs)  468 us
    pallas_call x5, Pallas kernels, mlp(): pl.pallas_call(ordered(functools.partial(mlp_kernel, n_in=len(bs), first=...  356 us
    pallas_call x5, Pallas kernels, flash(): pl.pallas_call(ordered(functools.partial(flash_kernel, q_src=q_src, kv_sr...  211 us
    pallas_call x6, Pallas kernels, qkv(): pl.pallas_call(ordered(functools.partial(qkv_kernel, n_in=n_in, n_q=n_q,...  97.6 us
    pallas_call x2, Pallas kernels, out_proj(): pl.pallas_call(ordered(functools.partial(out_kernel, blocks=blocks, n_w=l...  58.1 us
    ppermute x54, starting transfers between devices, send(): return lax.ppermute(v, *axis_pairs)  40 us
  transfers between devices with their start and end apart: 54, of which 28 were waited for; matrix products, arithmetic and copies ran while one was open for 3% of the time, Pallas kernels for 32%

profile of v11, /device:TPU:0, one launch (start us, length us, event | category | flops | bytes accessed | tf_op | source)
XLA Modules:
  0.0 1311.2 jit_solution(1995410400390343945)
XLA Ops:
  1.3 3.5 norm.4.refs_2_.refs_0_
  20.2 9.3 bitcast_dynamic-update-slice_fusion
  29.5 4.8 multiply_sine_fusion
  38.2 37.6 %qkv.6 = (bf16[8,1024,256]{2,1,0:T(8,128)(2,1)}, bf16[8,2,256,256]{3,2,1,0:T(8,128)(2,1)}) custom-call(bf16[256,4096]{1,0:T(8,128)(2,1)} %norm.4.refs_2_.refs_0_, bf16[256,4096]{1,0:T(8,128)(2,1)} %norm.5.refs_2_.refs_1_, bf16[256,4096]{1,0:T(8,128)(2,1)} %norm.6.refs_2_, bf16[256,4096]{1,0:T(8,128)(2,1)} %norm.7.refs_3_, ...), custom_call_target="tpu_custom_call" | custom-call | flops 25769803776 | bytes 12582912 | tf_op jit(solution)/shard_map/qkv/pallas_call | solution.py:127
  75.9 4.5 collective-permute-done.6.refs_1_
  80.4 14.0 %qkv.7 = (bf16[2,1024,256]{2,1,0:T(8,128)(2,1)}, bf16[2,2,256,256]{3,2,1,0:T(8,128)(2,1)}) custom-call(bf16[256,4096]{1,0:T(8,128)(2,1)} %collective-permute-done.5.refs_0_, bf16[256,4096]{1,0:T(8,128)(2,1)} %collective-permute-done.6.refs_1_, bf16[4096,1536]{1,0:T(8,128)(2,1)} %bitcast_dynamic-update-slice_fusion.1.refs_8_.refs_2_, ...), custom_call_target="tpu_custom_call" | custom-call | flops 6442450944 | bytes 12582912 | tf_op jit(solution)/shard_map/qkv/pallas_call | solution.py:127
  94.4 29.8 %collective-permute-done.4.refs_0_ = bf16[256,4096]{1,0:T(8,128)(2,1)} collective-permute-done((bf16[256,4096]{1,0:T(8,128)(2,1)}, bf16[256,4096]{1,0:T(8,128)(2,1)}, u32[]{:S(2)}, u32[]{:S(2)}) %collective-permute-start.4) | collective-permute-done | bytes 2097184 | tf_op jit(solution)/shard_map/ppermute | solution.py:713
  128.7 13.6 %qkv.8 = (bf16[2,1024,256]{2,1,0:T(8,128)(2,1)}, bf16[2,2,256,256]{3,2,1,0:T(8,128)(2,1)}) custom-call(bf16[256,4096]{1,0:T(8,128)(2,1)} %collective-permute-done.4.refs_0_, bf16[256,4096]{1,0:T(8,128)(2,1)} %collective-permute-done.7.refs_1_, bf16[4096,1536]{1,0:T(8,128)(2,1)} %bitcast_dynamic-update-slice_fusion.1.refs_8_.refs_2_, ...), custom_call_target="tpu_custom_call" | custom-call | flops 6442450944 | bytes 12582912 | tf_op jit(solution)/shard_map/qkv/pallas_call | solution.py:127
  142.3 50.0 %flash_part.1 = (f32[10,2,4,144,256]{4,3,2,1,0:T(8,128)}, bf16[256,4096]{1,0:T(8,128)(2,1)}, bf16[256,4096]{1,0:T(8,128)(2,1)}) custom-call(s32[845]{0:T(1024)} %dynamic-slice_reduce_fusion.refs_0_, bf16[8,1024,256]{2,1,0:T(8,128)(2,1)} %get-tuple-element.79.refs_1_, bf16[2,1024,256]{2,1,0:T(8,128)(2,1)} %get-tuple-element.86.refs_2_, ...), custom_call_target="tpu_custom_call" | custom-call | flops 38654705664 | bytes 3145728 | tf_op jit(solution)/shard_map/flash_part/pallas_call | solution.py:383
  197.7 13.7 %qkv.9 = (bf16[2,1024,256]{2,1,0:T(8,128)(2,1)}, bf16[2,2,256,256]{3,2,1,0:T(8,128)(2,1)}) custom-call(bf16[256,4096]{1,0:T(8,128)(2,1)} %collective-permute-done.8.refs_0_, bf16[256,4096]{1,0:T(8,128)(2,1)} %collective-permute-done.9.refs_1_, bf16[4096,1536]{1,0:T(8,128)(2,1)} %bitcast_dynamic-update-slice_fusion.1.refs_8_.refs_2_, ...), custom_call_target="tpu_custom_call" | custom-call | flops 6442450944 | bytes 12582912 | tf_op jit(solution)/shard_map/qkv/pallas_call | solution.py:127
  211.4 30.0 %collective-permute-done.10.refs_0_ = bf16[256,4096]{1,0:T(8,128)(2,1)} collective-permute-done((bf16[256,4096]{1,0:T(8,128)(2,1)}, bf16[256,4096]{1,0:T(8,128)(2,1)}, u32[]{:S(2)}, u32[]{:S(2)}) %collective-permute-start.10) | collective-permute-done | bytes 2097184 | tf_op jit(solution)/shard_map/ppermute | solution.py:713
  246.8 7.8 qkv.10.refs_5_.refs_7_
  256.3 10.8 qkv.11.refs_14_.refs_2_
  267.1 23.2 %collective-permute-done.12.refs_8_ = bf16[8,2,256,256]{3,2,1,0:T(8,128)(2,1)} collective-permute-done((bf16[8,2,256,256]{3,2,1,0:T(8,128)(2,1)}, bf16[8,2,256,256]{3,2,1,0:T(8,128)(2,1)}, u32[]{:S(2)}, u32[]{:S(2)}) %collective-permute-start.12) | collective-permute-done | bytes 2097184 | tf_op jit(solution)/shard_map/ppermute | solution.py:713
  290.3 11.2 collective-permute-done.13.refs_9_
  303.1 9.7 collective-permute-done.14.refs_10_
  314.3 9.7 collective-permute-done.15.refs_11_
  324.0 10.8 collective-permute-done.16.refs_12_
  334.7 29.1 %flash.4 = (bf16[2,256,1024]{2,1,0:T(8,128)(2,1)}, bf16[2,256,1024]{2,1,0:T(8,128)(2,1)}, bf16[2,256,1024]{2,1,0:T(8,128)(2,1)}, bf16[2,256,1024]{2,1,0:T(8,128)(2,1)}, f32[8,128]{1,0:T(8,128)}) custom-call(s32[845]{0:T(1024)} %dynamic-slice_reduce_fusion.refs_0_, bf16[8,1024,256]{2,1,0:T(8,128)(2,1)} %get-tuple-element.79.refs_1_, ...), custom_call_target="tpu_custom_call" | custom-call | flops 23622320128 | bytes 8388608 | tf_op jit(solution)/shard_map/flash/pallas_call | solution.py:383
  364.8 43.9 %flash.5 = (bf16[2,256,1024]{2,1,0:T(8,128)(2,1)}, bf16[2,256,1024]{2,1,0:T(8,128)(2,1)}, bf16[2,256,1024]{2,1,0:T(8,128)(2,1)}, bf16[2,256,1024]{2,1,0:T(8,128)(2,1)}, f32[8,128]{1,0:T(8,128)}) custom-call(s32[845]{0:T(1024)} %dynamic-slice_reduce_fusion.refs_0_, ...), custom_call_target="tpu_custom_call", output_to_operand_aliasing={{0}: (14, {}), {1}: (15, {}), {2}: (16, {}), {3}: (17, {})} | custom-call | flops 32212254720 | bytes 8388608 | tf_op jit(solution)/shard_map/flash/pallas_call | solution.py:383
  412.3 43.8 %flash.6 = (bf16[2,256,1024]{2,1,0:T(8,128)(2,1)}, bf16[2,256,1024]{2,1,0:T(8,128)(2,1)}, bf16[2,256,1024]{2,1,0:T(8,128)(2,1)}, bf16[2,256,1024]{2,1,0:T(8,128)(2,1)}, f32[8,128]{1,0:T(8,128)}) custom-call(s32[845]{0:T(1024)} %dynamic-slice_reduce_fusion.refs_0_, bf16[8,1024,256]{2,1,0:T(8,128)(2,1)} %get-tuple-element.79.refs_1_, ...), custom_call_target="tpu_custom_call" | custom-call | flops 32212254720 | bytes 8388608 | tf_op jit(solution)/shard_map/flash/pallas_call | solution.py:383
  459.8 3.5 collective-permute-done.25.refs_10_
  472.3 29.0 %outp.2 = (bf16[256,4096]{1,0:T(8,128)(2,1)}, bf16[256,4096]{1,0:T(8,128)(2,1)}, bf16[256,4096]{1,0:T(8,128)(2,1)}, bf16[256,4096]{1,0:T(8,128)(2,1)}) custom-call(bf16[2,256,1024]{2,1,0:T(8,128)(2,1)} %get-tuple-element.96.refs_0_, bf16[2,256,1024]{2,1,0:T(8,128)(2,1)} %collective-permute-done.17.refs_1_, ...), custom_call_target="tpu_custom_call" | custom-call | flops 17179869184 | bytes 33554432 | tf_op jit(solution)/shard_map/outp/pallas_call | solution.py:492
  501.5 7.4 collective-permute-start.29
  508.9 43.9 %flash.7 = (bf16[2,256,1024]{2,1,0:T(8,128)(2,1)}, bf16[2,256,1024]{2,1,0:T(8,128)(2,1)}, bf16[2,256,1024]{2,1,0:T(8,128)(2,1)}, bf16[2,256,1024]{2,1,0:T(8,128)(2,1)}, f32[8,128]{1,0:T(8,128)}) custom-call(s32[845]{0:T(1024)} %dynamic-slice_reduce_fusion.refs_0_, ...), custom_call_target="tpu_custom_call", output_to_operand_aliasing={{0}: (14, {}), {1}: (15, {}), {2}: (16, {}), {3}: (17, {})} | custom-call | flops 32212254720 | bytes 8388608 | tf_op jit(solution)/shard_map/flash/pallas_call | solution.py:383
  555.4 4.5 collective-permute-done.31.refs_3_
  559.9 86.7 %mlp.5 = (bf16[512,4096]{1,0:T(8,128)(2,1)}, bf16[512,4096]{1,0:T(8,128)(2,1)}) custom-call(bf16[256,4096]{1,0:T(8,128)(2,1)} %get-tuple-element.110.refs_0_, bf16[256,4096]{1,0:T(8,128)(2,1)} %collective-permute-done.29.refs_1_, bf16[256,4096]{1,0:T(8,128)(2,1)} %collective-permute-done.30.refs_2_, bf16[256,4096]{1,0:T(8,128)(2,1)} %collective-permute-done.31.refs_3_, ...), custom_call_target="tpu_custom_call" | custom-call | flops 77309411328 | bytes 75497472 | tf_op jit(solution)/shard_map/mlp/pallas_call | solution.py:577
  650.4 45.2 %collective-permute-done.37.refs_1_ = bf16[256,4096]{1,0:T(8,128)(2,1)} collective-permute-done((bf16[256,4096]{1,0:T(8,128)(2,1)}, bf16[256,4096]{1,0:T(8,128)(2,1)}, u32[]{:S(2)}, u32[]{:S(2)}) %collective-permute-start.37) | collective-permute-done | bytes 2097184 | tf_op jit(solution)/shard_map/ppermute | solution.py:713
  696.1 22.0 %collective-permute-done.34.refs_2_ = bf16[2,256,1024]{2,1,0:T(8,128)(2,1)} collective-permute-done((bf16[2,256,1024]{2,1,0:T(8,128)(2,1)}, bf16[2,256,1024]{2,1,0:T(8,128)(2,1)}, u32[]{:S(2)}, u32[]{:S(2)}) %collective-permute-start.34) | collective-permute-done | bytes 1048608 | tf_op jit(solution)/shard_map/ppermute | solution.py:713
  718.1 21.3 %collective-permute-done.35.refs_3_ = bf16[2,256,1024]{2,1,0:T(8,128)(2,1)} collective-permute-done((bf16[2,256,1024]{2,1,0:T(8,128)(2,1)}, bf16[2,256,1024]{2,1,0:T(8,128)(2,1)}, u32[]{:S(2)}, u32[]{:S(2)}) %collective-permute-start.35) | collective-permute-done | bytes 1048608 | tf_op jit(solution)/shard_map/ppermute | solution.py:713
  739.4 29.0 %outp.3 = (bf16[256,4096]{1,0:T(8,128)(2,1)}, bf16[256,4096]{1,0:T(8,128)(2,1)}, bf16[256,4096]{1,0:T(8,128)(2,1)}, bf16[256,4096]{1,0:T(8,128)(2,1)}) custom-call(bf16[2,256,1024]{2,1,0:T(8,128)(2,1)} %get-tuple-element.120.refs_0_, bf16[2,256,1024]{2,1,0:T(8,128)(2,1)} %collective-permute-done.33.refs_1_, ...), custom_call_target="tpu_custom_call" | custom-call | flops 17179869184 | bytes 33554432 | tf_op jit(solution)/shard_map/outp/pallas_call | solution.py:492
  768.4 4.3 add_convert_fusion.2.refs_7_
  772.8 86.9 %mlp.6 = (bf16[512,4096]{1,0:T(8,128)(2,1)}, bf16[512,4096]{1,0:T(8,128)(2,1)}) custom-call(bf16[256,4096]{1,0:T(8,128)(2,1)} %get-tuple-element.126.refs_0_, bf16[256,4096]{1,0:T(8,128)(2,1)} %collective-permute-done.37.refs_1_, bf16[256,4096]{1,0:T(8,128)(2,1)} %collective-permute-done.38.refs_2_, bf16[256,4096]{1,0:T(8,128)(2,1)} %collective-permute-done.39.refs_3_, ...), custom_call_target="tpu_custom_call" | custom-call | flops 77309411328 | bytes 75497472 | tf_op jit(solution)/shard_map/mlp/pallas_call | solution.py:577
  862.2 46.8 %collective-permute-done.42.refs_1_ = bf16[256,4096]{1,0:T(8,128)(2,1)} collective-permute-done((bf16[256,4096]{1,0:T(8,128)(2,1)}, bf16[256,4096]{1,0:T(8,128)(2,1)}, u32[]{:S(2)}, u32[]{:S(2)}) %collective-permute-start.42) | collective-permute-done | bytes 2097184 | tf_op jit(solution)/shard_map/ppermute | solution.py:713
  909.0 44.1 %collective-permute-done.36.refs_2_ = bf16[256,4096]{1,0:T(8,128)(2,1)} collective-permute-done((bf16[256,4096]{1,0:T(8,128)(2,1)}, bf16[256,4096]{1,0:T(8,128)(2,1)}, u32[]{:S(2)}, u32[]{:S(2)}) %collective-permute-start.36) | collective-permute-done | bytes 2097184 | tf_op jit(solution)/shard_map/ppermute | solution.py:713
  953.0 5.6 zsum.5.refs_0_
  958.6 4.4 add_convert_fusion.1.refs_7_
  963.0 86.8 %mlp.7 = (bf16[512,4096]{1,0:T(8,128)(2,1)}, bf16[512,4096]{1,0:T(8,128)(2,1)}) custom-call(bf16[256,4096]{1,0:T(8,128)(2,1)} %get-tuple-element.132.refs_0_, bf16[256,4096]{1,0:T(8,128)(2,1)} %collective-permute-done.42.refs_1_, bf16[256,4096]{1,0:T(8,128)(2,1)} %collective-permute-done.43.refs_2_, bf16[256,4096]{1,0:T(8,128)(2,1)} %collective-permute-done.44.refs_3_, ...), custom_call_target="tpu_custom_call" | custom-call | flops 77309411328 | bytes 75497472 | tf_op jit(solution)/shard_map/mlp/pallas_call | solution.py:577
  1051.9 46.8 %collective-permute-done.47.refs_1_ = bf16[256,4096]{1,0:T(8,128)(2,1)} collective-permute-done((bf16[256,4096]{1,0:T(8,128)(2,1)}, bf16[256,4096]{1,0:T(8,128)(2,1)}, u32[]{:S(2)}, u32[]{:S(2)}) %collective-permute-start.47) | collective-permute-done | bytes 2097184 | tf_op jit(solution)/shard_map/ppermute | solution.py:713
  1098.6 44.4 %collective-permute-done.41.refs_3_ = bf16[256,4096]{1,0:T(8,128)(2,1)} collective-permute-done((bf16[256,4096]{1,0:T(8,128)(2,1)}, bf16[256,4096]{1,0:T(8,128)(2,1)}, u32[]{:S(2)}, u32[]{:S(2)}) %collective-permute-start.41) | collective-permute-done | bytes 2097184 | tf_op jit(solution)/shard_map/ppermute | solution.py:713
  1143.1 5.8 zsum.6.refs_0_
  1148.9 4.3 add_convert_fusion.refs_7_
  1154.9 48.0 %mlp.8 = (bf16[256,4096]{1,0:T(8,128)(2,1)}, bf16[256,4096]{1,0:T(8,128)(2,1)}) custom-call(bf16[256,4096]{1,0:T(8,128)(2,1)} %get-tuple-element.137.refs_0_, bf16[256,4096]{1,0:T(8,128)(2,1)} %collective-permute-done.47.refs_1_, bf16[256,4096]{1,0:T(8,128)(2,1)} %collective-permute-done.48.refs_2_, bf16[256,4096]{1,0:T(8,128)(2,1)} %collective-permute-done.49.refs_3_, ...), custom_call_target="tpu_custom_call" | custom-call | flops 38654705664 | bytes 75497472 | tf_op jit(solution)/shard_map/mlp/pallas_call | solution.py:577
  1203.0 5.6 zsum.7.refs_0_
  1211.4 47.9 %mlp.9 = (bf16[256,4096]{1,0:T(8,128)(2,1)}, bf16[256,4096]{1,0:T(8,128)(2,1)}) custom-call(bf16[256,4096]{1,0:T(8,128)(2,1)} %get-tuple-element.137.refs_0_, bf16[256,4096]{1,0:T(8,128)(2,1)} %collective-permute-done.47.refs_1_, bf16[256,4096]{1,0:T(8,128)(2,1)} %collective-permute-done.48.refs_2_, bf16[256,4096]{1,0:T(8,128)(2,1)} %collective-permute-done.49.refs_3_, ...), custom_call_target="tpu_custom_call" | custom-call | flops 38654705664 | bytes 75497472 | tf_op jit(solution)/shard_map/mlp/pallas_call | solution.py:577
  1260.2 3.6 collective-permute-done.52.refs_2_
  1268.0 18.1 %collective-permute-done.51.refs_3_ = bf16[128,4096]{1,0:T(8,128)(2,1)} collective-permute-done((bf16[128,4096]{1,0:T(8,128)(2,1)}, bf16[128,4096]{1,0:T(8,128)(2,1)}, u32[]{:S(2)}, u32[]{:S(2)}) %collective-permute-start.51) | collective-permute-done | bytes 1048608 | tf_op jit(solution)/shard_map/ppermute | solution.py:713
  1289.4 18.3 %collective-permute-done.53.refs_3_ = bf16[128,4096]{1,0:T(8,128)(2,1)} collective-permute-done((bf16[128,4096]{1,0:T(8,128)(2,1)}, bf16[128,4096]{1,0:T(8,128)(2,1)}, u32[]{:S(2)}, u32[]{:S(2)}) %collective-permute-start.53) | collective-permute-done | bytes 1048608 | tf_op jit(solution)/shard_map/ppermute | solution.py:713
  (108 shorter events, 85.5 us)
Async XLA Ops:
  4.8 71.0 %collective-permute-start.5 = (bf16[256,4096]{1,0:T(8,128)(2,1)}, bf16[256,4096]{1,0:T(8,128)(2,1)}, u32[]{:S(2)}, u32[]{:S(2)}) collective-permute-start(bf16[256,4096]{1,0:T(8,128)(2,1)} %norm.4.refs_2_.refs_0_), channel_id=1, source_target_pairs={{0,2},{1,3},{2,0},{3,1},{4,6},{5,7},{6,4},{7,5}} | collective-permute-start | bytes 6291464 | tf_op jit(solution)/shard_map/ppermute | solution.py:713
  8.1 30.1 %collective-permute-start = (bf16[256,4096]{1,0:T(8,128)(2,1)}, bf16[256,4096]{1,0:T(8,128)(2,1)}, u32[]{:S(2)}, u32[]{:S(2)}) collective-permute-start(bf16[256,4096]{1,0:T(8,128)(2,1)} %norm.4.refs_2_.refs_0_), channel_id=1, source_target_pairs={{0,1},{1,0},{2,3},{3,2},{4,5},{5,4},{6,7},{7,6}} | collective-permute-start | bytes 6291464 | tf_op jit(solution)/shard_map/ppermute | solution.py:713
  11.6 26.7 %collective-permute-start.1 = (bf16[256,4096]{1,0:T(8,128)(2,1)}, bf16[256,4096]{1,0:T(8,128)(2,1)}, u32[]{:S(2)}, u32[]{:S(2)}) collective-permute-start(bf16[256,4096]{1,0:T(8,128)(2,1)} %norm.5.refs_2_.refs_1_), channel_id=1, source_target_pairs={{0,1},{1,0},{2,3},{3,2},{4,5},{5,4},{6,7},{7,6}} | collective-permute-start | bytes 6291464 | tf_op jit(solution)/shard_map/ppermute | solution.py:713
  15.5 22.7 %collective-permute-start.2 = (bf16[256,4096]{1,0:T(8,128)(2,1)}, bf16[256,4096]{1,0:T(8,128)(2,1)}, u32[]{:S(2)}, u32[]{:S(2)}) collective-permute-start(bf16[256,4096]{1,0:T(8,128)(2,1)} %norm.6.refs_2_), channel_id=1, source_target_pairs={{0,1},{1,0},{2,3},{3,2},{4,5},{5,4},{6,7},{7,6}} | collective-permute-start | bytes 6291464 | tf_op jit(solution)/shard_map/ppermute | solution.py:713
  18.9 19.3 %collective-permute-start.3 = (bf16[256,4096]{1,0:T(8,128)(2,1)}, bf16[256,4096]{1,0:T(8,128)(2,1)}, u32[]{:S(2)}, u32[]{:S(2)}) collective-permute-start(bf16[256,4096]{1,0:T(8,128)(2,1)} %norm.7.refs_3_), channel_id=1, source_target_pairs={{0,1},{1,0},{2,3},{3,2},{4,5},{5,4},{6,7},{7,6}} | collective-permute-start | bytes 6291464 | tf_op jit(solution)/shard_map/ppermute | solution.py:713
  75.9 48.3 %collective-permute-start.4 = (bf16[256,4096]{1,0:T(8,128)(2,1)}, bf16[256,4096]{1,0:T(8,128)(2,1)}, u32[]{:S(2)}, u32[]{:S(2)}) collective-permute-start(bf16[256,4096]{1,0:T(8,128)(2,1)} %norm.5.refs_2_.refs_1_), channel_id=1, source_target_pairs={{0,2},{1,3},{2,0},{3,1},{4,6},{5,7},{6,4},{7,5}} | collective-permute-start | bytes 6291464 | tf_op jit(solution)/shard_map/ppermute | solution.py:713
  124.2 68.1 %collective-permute-start.8 = (bf16[256,4096]{1,0:T(8,128)(2,1)}, bf16[256,4096]{1,0:T(8,128)(2,1)}, u32[]{:S(2)}, u32[]{:S(2)}) collective-permute-start(bf16[256,4096]{1,0:T(8,128)(2,1)} %norm.6.refs_2_), channel_id=1, source_target_pairs={{0,2},{1,3},{2,0},{3,1},{4,6},{5,7},{6,4},{7,5}} | collective-permute-start | bytes 6291464 | tf_op jit(solution)/shard_map/ppermute | solution.py:713
  193.5 47.9 %collective-permute-start.10 = (bf16[256,4096]{1,0:T(8,128)(2,1)}, bf16[256,4096]{1,0:T(8,128)(2,1)}, u32[]{:S(2)}, u32[]{:S(2)}) collective-permute-start(bf16[256,4096]{1,0:T(8,128)(2,1)} %norm.7.refs_3_), channel_id=1, source_target_pairs={{0,2},{1,3},{2,0},{3,1},{4,6},{5,7},{6,4},{7,5}} | collective-permute-start | bytes 6291464 | tf_op jit(solution)/shard_map/ppermute | solution.py:713
  241.4 5.4 collective-permute-start.11
  241.4 48.8 %collective-permute-start.12 = (bf16[8,2,256,256]{3,2,1,0:T(8,128)(2,1)}, bf16[8,2,256,256]{3,2,1,0:T(8,128)(2,1)}, u32[]{:S(2)}, u32[]{:S(2)}) collective-permute-start(bf16[8,2,256,256]{3,2,1,0:T(8,128)(2,1)} %get-tuple-element.80.refs_5_.refs_3_), channel_id=1, source_target_pairs={{0,4},{4,0},{1,5},{5,1},{2,6},{6,2},{3,7},{7,3}} | collective-permute-start | bytes 6291464 | tf_op jit(solution)/shard_map/ppermute | solution.py:713
  244.3 57.2 %collective-permute-start.13 = (bf16[2,2,256,256]{3,2,1,0:T(8,128)(2,1)}, bf16[2,2,256,256]{3,2,1,0:T(8,128)(2,1)}, u32[]{:S(2)}, u32[]{:S(2)}) collective-permute-start(bf16[2,2,256,256]{3,2,1,0:T(8,128)(2,1)} %get-tuple-element.82.refs_5_.refs_4_), channel_id=1, source_target_pairs={{0,4},{4,0},{1,5},{5,1},{2,6},{6,2},{3,7},{7,3}} | collective-permute-start | bytes 1572872 | tf_op jit(solution)/shard_map/ppermute | solution.py:713
  244.8 68.0 %collective-permute-start.14 = (bf16[2,2,256,256]{3,2,1,0:T(8,128)(2,1)}, bf16[2,2,256,256]{3,2,1,0:T(8,128)(2,1)}, u32[]{:S(2)}, u32[]{:S(2)}) collective-permute-start(bf16[2,2,256,256]{3,2,1,0:T(8,128)(2,1)} %get-tuple-element.85.refs_5_), channel_id=1, source_target_pairs={{0,4},{4,0},{1,5},{5,1},{2,6},{6,2},{3,7},{7,3}} | collective-permute-start | bytes 1572872 | tf_op jit(solution)/shard_map/ppermute | solution.py:713
  246.4 77.6 %collective-permute-start.15 = (bf16[2,2,256,256]{3,2,1,0:T(8,128)(2,1)}, bf16[2,2,256,256]{3,2,1,0:T(8,128)(2,1)}, u32[]{:S(2)}, u32[]{:S(2)}) collective-permute-start(bf16[2,2,256,256]{3,2,1,0:T(8,128)(2,1)} %get-tuple-element.89.refs_5_.refs_6_), channel_id=1, source_target_pairs={{0,4},{4,0},{1,5},{5,1},{2,6},{6,2},{3,7},{7,3}} | collective-permute-start | bytes 1572872 | tf_op jit(solution)/shard_map/ppermute | solution.py:713
  254.6 80.1 %collective-permute-start.16 = (bf16[2,2,256,256]{3,2,1,0:T(8,128)(2,1)}, bf16[2,2,256,256]{3,2,1,0:T(8,128)(2,1)}, u32[]{:S(2)}, u32[]{:S(2)}) collective-permute-start(bf16[2,2,256,256]{3,2,1,0:T(8,128)(2,1)} %qkv.10.refs_5_.refs_7_), channel_id=1, source_target_pairs={{0,4},{4,0},{1,5},{5,1},{2,6},{6,2},{3,7},{7,3}} | collective-permute-start | bytes 1572872 | tf_op jit(solution)/shard_map/ppermute | solution.py:713
  290.2 176.1 %collective-permute-start.20 = (bf16[1024,4096]{1,0:T(8,128)(2,1)}, bf16[1024,4096]{1,0:T(8,128)(2,1)}, u32[]{:S(2)}, u32[]{:S(2)}) collective-permute-start(bf16[1024,4096]{1,0:T(8,128)(2,1)} %bitcast.24), channel_id=1, source_target_pairs={{0,1},{1,0},{2,3},{3,2},{4,5},{5,4},{6,7},{7,6}} | collective-permute-start | bytes 25165832 | tf_op jit(solution)/shard_map/ppermute | solution.py:713
  301.5 62.3 %collective-permute-start.21 = (bf16[256,4096]{1,0:T(8,128)(2,1)}, bf16[256,4096]{1,0:T(8,128)(2,1)}, u32[]{:S(2)}, u32[]{:S(2)}) collective-permute-start(bf16[256,4096]{1,0:T(8,128)(2,1)} %get-tuple-element.101), channel_id=1, source_target_pairs={{0,2},{1,3},{2,0},{3,1},{4,6},{5,7},{6,4},{7,5}} | collective-permute-start | bytes 6291464 | tf_op jit(solution)/shard_map/ppermute | solution.py:713
  312.7 96.0 %collective-permute-start.22 = (bf16[256,4096]{1,0:T(8,128)(2,1)}, bf16[256,4096]{1,0:T(8,128)(2,1)}, u32[]{:S(2)}, u32[]{:S(2)}) collective-permute-start(bf16[256,4096]{1,0:T(8,128)(2,1)} %get-tuple-element.103), channel_id=1, source_target_pairs={{0,2},{1,3},{2,0},{3,1},{4,6},{5,7},{6,4},{7,5}} | collective-permute-start | bytes 6291464 | tf_op jit(solution)/shard_map/ppermute | solution.py:713
  363.8 47.5 %collective-permute-start.23 = (bf16[256,4096]{1,0:T(8,128)(2,1)}, bf16[256,4096]{1,0:T(8,128)(2,1)}, u32[]{:S(2)}, u32[]{:S(2)}) collective-permute-start(bf16[256,4096]{1,0:T(8,128)(2,1)} %collective-permute-done.21.refs_6_), channel_id=1, source_target_pairs={{0,4},{4,0},{1,5},{5,1},{2,6},{6,2},{3,7},{7,3}} | collective-permute-start | bytes 6291464 | tf_op jit(solution)/shard_map/ppermute | solution.py:713
  408.8 50.1 %collective-permute-start.17 = (bf16[2,256,1024]{2,1,0:T(8,128)(2,1)}, bf16[2,256,1024]{2,1,0:T(8,128)(2,1)}, u32[]{:S(2)}, u32[]{:S(2)}) collective-permute-start(bf16[2,256,1024]{2,1,0:T(8,128)(2,1)} %get-tuple-element.97), channel_id=1, source_target_pairs={{0,1},{1,0},{2,3},{3,2},{4,5},{5,4},{6,7},{7,6}} | collective-permute-start | bytes 3145736 | tf_op jit(solution)/shard_map/ppermute | solution.py:713
  408.8 50.5 %collective-permute-start.18 = (bf16[2,256,1024]{2,1,0:T(8,128)(2,1)}, bf16[2,256,1024]{2,1,0:T(8,128)(2,1)}, u32[]{:S(2)}, u32[]{:S(2)}) collective-permute-start(bf16[2,256,1024]{2,1,0:T(8,128)(2,1)} %get-tuple-element.98), channel_id=1, source_target_pairs={{0,2},{1,3},{2,0},{3,1},{4,6},{5,7},{6,4},{7,5}} | collective-permute-start | bytes 3145736 | tf_op jit(solution)/shard_map/ppermute | solution.py:713
  409.6 49.8 %collective-permute-start.19 = (bf16[2,256,1024]{2,1,0:T(8,128)(2,1)}, bf16[2,256,1024]{2,1,0:T(8,128)(2,1)}, u32[]{:S(2)}, u32[]{:S(2)}) collective-permute-start(bf16[2,256,1024]{2,1,0:T(8,128)(2,1)} %get-tuple-element.99), channel_id=1, source_target_pairs={{0,3},{1,2},{2,1},{3,0},{4,7},{5,6},{6,5},{7,4}} | collective-permute-start | bytes 3145736 | tf_op jit(solution)/shard_map/ppermute | solution.py:713
  411.3 47.5 %collective-permute-start.24 = (bf16[256,4096]{1,0:T(8,128)(2,1)}, bf16[256,4096]{1,0:T(8,128)(2,1)}, u32[]{:S(2)}, u32[]{:S(2)}) collective-permute-start(bf16[256,4096]{1,0:T(8,128)(2,1)} %collective-permute-done.22.refs_7_), channel_id=1, source_target_pairs={{0,4},{4,0},{1,5},{5,1},{2,6},{6,2},{3,7},{7,3}} | collective-permute-start | bytes 6291464 | tf_op jit(solution)/shard_map/ppermute | solution.py:713
  458.8 7.5 collective-permute-start.26
  459.3 10.0 collective-permute-start.27
  459.4 13.0 collective-permute-start.28
  501.3 54.1 %collective-permute-start.30 = (bf16[256,4096]{1,0:T(8,128)(2,1)}, bf16[256,4096]{1,0:T(8,128)(2,1)}, u32[]{:S(2)}, u32[]{:S(2)}) collective-permute-start(bf16[256,4096]{1,0:T(8,128)(2,1)} %get-tuple-element.110.refs_0_), channel_id=1, source_target_pairs={{0,1},{1,0},{2,3},{3,2},{4,5},{5,4},{6,7},{7,6}} | collective-permute-start | bytes 6291464 | tf_op jit(solution)/shard_map/ppermute | solution.py:713
  501.5 53.9 %collective-permute-start.29 = (bf16[256,4096]{1,0:T(8,128)(2,1)}, bf16[256,4096]{1,0:T(8,128)(2,1)}, u32[]{:S(2)}, u32[]{:S(2)}) collective-permute-start(bf16[256,4096]{1,0:T(8,128)(2,1)} %get-tuple-element.110.refs_0_), channel_id=1, source_target_pairs={{0,2},{1,3},{2,0},{3,1},{4,6},{5,7},{6,4},{7,5}} | collective-permute-start | bytes 6291464 | tf_op jit(solution)/shard_map/ppermute | solution.py:713
  646.6 121.8 %collective-permute-start.32 = (bf16[512,4096]{1,0:T(8,128)(2,1)}, bf16[512,4096]{1,0:T(8,128)(2,1)}, u32[]{:S(2)}, u32[]{:S(2)}) collective-permute-start(bf16[512,4096]{1,0:T(8,128)(2,1)} %get-tuple-element.119), channel_id=1, source_target_pairs={{0,1},{1,0},{2,3},{3,2},{4,5},{5,4},{6,7},{7,6}} | collective-permute-start | bytes 12582920 | tf_op jit(solution)/shard_map/ppermute | solution.py:713
  646.8 48.8 %collective-permute-start.37 = (bf16[256,4096]{1,0:T(8,128)(2,1)}, bf16[256,4096]{1,0:T(8,128)(2,1)}, u32[]{:S(2)}, u32[]{:S(2)}) collective-permute-start(bf16[256,4096]{1,0:T(8,128)(2,1)} %get-tuple-element.126.refs_0_), channel_id=1, source_target_pairs={{0,2},{1,3},{2,0},{3,1},{4,6},{5,7},{6,4},{7,5}} | collective-permute-start | bytes 6291464 | tf_op jit(solution)/shard_map/ppermute | solution.py:713
  648.5 47.1 %collective-permute-start.33 = (bf16[2,256,1024]{2,1,0:T(8,128)(2,1)}, bf16[2,256,1024]{2,1,0:T(8,128)(2,1)}, u32[]{:S(2)}, u32[]{:S(2)}) collective-permute-start(bf16[2,256,1024]{2,1,0:T(8,128)(2,1)} %get-tuple-element.121), channel_id=1, source_target_pairs={{0,1},{1,0},{2,3},{3,2},{4,5},{5,4},{6,7},{7,6}} | collective-permute-start | bytes 3145736 | tf_op jit(solution)/shard_map/ppermute | solution.py:713
  648.6 69.4 %collective-permute-start.34 = (bf16[2,256,1024]{2,1,0:T(8,128)(2,1)}, bf16[2,256,1024]{2,1,0:T(8,128)(2,1)}, u32[]{:S(2)}, u32[]{:S(2)}) collective-permute-start(bf16[2,256,1024]{2,1,0:T(8,128)(2,1)} %get-tuple-element.122), channel_id=1, source_target_pairs={{0,2},{1,3},{2,0},{3,1},{4,6},{5,7},{6,4},{7,5}} | collective-permute-start | bytes 3145736 | tf_op jit(solution)/shard_map/ppermute | solution.py:713
  648.9 90.5 %collective-permute-start.35 = (bf16[2,256,1024]{2,1,0:T(8,128)(2,1)}, bf16[2,256,1024]{2,1,0:T(8,128)(2,1)}, u32[]{:S(2)}, u32[]{:S(2)}) collective-permute-start(bf16[2,256,1024]{2,1,0:T(8,128)(2,1)} %get-tuple-element.123), channel_id=1, source_target_pairs={{0,3},{1,2},{2,1},{3,0},{4,7},{5,6},{6,5},{7,4}} | collective-permute-start | bytes 3145736 | tf_op jit(solution)/shard_map/ppermute | solution.py:713
  695.6 77.2 %collective-permute-start.38 = (bf16[256,4096]{1,0:T(8,128)(2,1)}, bf16[256,4096]{1,0:T(8,128)(2,1)}, u32[]{:S(2)}, u32[]{:S(2)}) collective-permute-start(bf16[256,4096]{1,0:T(8,128)(2,1)} %get-tuple-element.126.refs_0_), channel_id=1, source_target_pairs={{0,1},{1,0},{2,3},{3,2},{4,5},{5,4},{6,7},{7,6}} | collective-permute-start | bytes 6291464 | tf_op jit(solution)/shard_map/ppermute | solution.py:713
  695.6 77.2 %collective-permute-start.39 = (bf16[256,4096]{1,0:T(8,128)(2,1)}, bf16[256,4096]{1,0:T(8,128)(2,1)}, u32[]{:S(2)}, u32[]{:S(2)}) collective-permute-start(bf16[256,4096]{1,0:T(8,128)(2,1)} %collective-permute-done.37.refs_1_), channel_id=1, source_target_pairs={{0,1},{1,0},{2,3},{3,2},{4,5},{5,4},{6,7},{7,6}} | collective-permute-start | bytes 6291464 | tf_op jit(solution)/shard_map/ppermute | solution.py:713
  859.7 98.9 %collective-permute-start.40 = (bf16[512,4096]{1,0:T(8,128)(2,1)}, bf16[512,4096]{1,0:T(8,128)(2,1)}, u32[]{:S(2)}, u32[]{:S(2)}) collective-permute-start(bf16[512,4096]{1,0:T(8,128)(2,1)} %get-tuple-element.129), channel_id=1, source_target_pairs={{0,1},{1,0},{2,3},{3,2},{4,5},{5,4},{6,7},{7,6}} | collective-permute-start | bytes 12582920 | tf_op jit(solution)/shard_map/ppermute | solution.py:713
  860.1 48.8 %collective-permute-start.42 = (bf16[256,4096]{1,0:T(8,128)(2,1)}, bf16[256,4096]{1,0:T(8,128)(2,1)}, u32[]{:S(2)}, u32[]{:S(2)}) collective-permute-start(bf16[256,4096]{1,0:T(8,128)(2,1)} %get-tuple-element.132.refs_0_), channel_id=1, source_target_pairs={{0,2},{1,3},{2,0},{3,1},{4,6},{5,7},{6,4},{7,5}} | collective-permute-start | bytes 6291464 | tf_op jit(solution)/shard_map/ppermute | solution.py:713
  861.9 91.2 %collective-permute-start.36 = (bf16[256,4096]{1,0:T(8,128)(2,1)}, bf16[256,4096]{1,0:T(8,128)(2,1)}, u32[]{:S(2)}, u32[]{:S(2)}) collective-permute-start(bf16[256,4096]{1,0:T(8,128)(2,1)} %add_convert_fusion.2.refs_7_), channel_id=1, source_target_pairs={{0,2},{1,3},{2,0},{3,1},{4,6},{5,7},{6,4},{7,5}} | collective-permute-start | bytes 6291464 | tf_op jit(solution)/shard_map/ppermute | solution.py:713
  862.2 100.8 %collective-permute-start.43 = (bf16[256,4096]{1,0:T(8,128)(2,1)}, bf16[256,4096]{1,0:T(8,128)(2,1)}, u32[]{:S(2)}, u32[]{:S(2)}) collective-permute-start(bf16[256,4096]{1,0:T(8,128)(2,1)} %get-tuple-element.132.refs_0_), channel_id=1, source_target_pairs={{0,1},{1,0},{2,3},{3,2},{4,5},{5,4},{6,7},{7,6}} | collective-permute-start | bytes 6291464 | tf_op jit(solution)/shard_map/ppermute | solution.py:713
  909.0 54.0 %collective-permute-start.44 = (bf16[256,4096]{1,0:T(8,128)(2,1)}, bf16[256,4096]{1,0:T(8,128)(2,1)}, u32[]{:S(2)}, u32[]{:S(2)}) collective-permute-start(bf16[256,4096]{1,0:T(8,128)(2,1)} %collective-permute-done.42.refs_1_), channel_id=1, source_target_pairs={{0,1},{1,0},{2,3},{3,2},{4,5},{5,4},{6,7},{7,6}} | collective-permute-start | bytes 6291464 | tf_op jit(solution)/shard_map/ppermute | solution.py:713
  1049.8 99.1 %collective-permute-start.45 = (bf16[512,4096]{1,0:T(8,128)(2,1)}, bf16[512,4096]{1,0:T(8,128)(2,1)}, u32[]{:S(2)}, u32[]{:S(2)}) collective-permute-start(bf16[512,4096]{1,0:T(8,128)(2,1)} %get-tuple-element.135), channel_id=1, source_target_pairs={{0,1},{1,0},{2,3},{3,2},{4,5},{5,4},{6,7},{7,6}} | collective-permute-start | bytes 12582920 | tf_op jit(solution)/shard_map/ppermute | solution.py:713
  1049.8 48.8 %collective-permute-start.47 = (bf16[256,4096]{1,0:T(8,128)(2,1)}, bf16[256,4096]{1,0:T(8,128)(2,1)}, u32[]{:S(2)}, u32[]{:S(2)}) collective-permute-start(bf16[256,4096]{1,0:T(8,128)(2,1)} %get-tuple-element.137.refs_0_), channel_id=1, source_target_pairs={{0,2},{1,3},{2,0},{3,1},{4,6},{5,7},{6,4},{7,5}} | collective-permute-start | bytes 6291464 | tf_op jit(solution)/shard_map/ppermute | solution.py:713
  1051.5 91.6 %collective-permute-start.41 = (bf16[256,4096]{1,0:T(8,128)(2,1)}, bf16[256,4096]{1,0:T(8,128)(2,1)}, u32[]{:S(2)}, u32[]{:S(2)}) collective-permute-start(bf16[256,4096]{1,0:T(8,128)(2,1)} %add_convert_fusion.1.refs_7_), channel_id=1, source_target_pairs={{0,2},{1,3},{2,0},{3,1},{4,6},{5,7},{6,4},{7,5}} | collective-permute-start | bytes 6291464 | tf_op jit(solution)/shard_map/ppermute | solution.py:713
  1051.9 103.0 %collective-permute-start.48 = (bf16[256,4096]{1,0:T(8,128)(2,1)}, bf16[256,4096]{1,0:T(8,128)(2,1)}, u32[]{:S(2)}, u32[]{:S(2)}) collective-permute-start(bf16[256,4096]{1,0:T(8,128)(2,1)} %get-tuple-element.137.refs_0_), channel_id=1, source_target_pairs={{0,1},{1,0},{2,3},{3,2},{4,5},{5,4},{6,7},{7,6}} | collective-permute-start | bytes 6291464 | tf_op jit(solution)/shard_map/ppermute | solution.py:713
  1098.6 56.2 %collective-permute-start.49 = (bf16[256,4096]{1,0:T(8,128)(2,1)}, bf16[256,4096]{1,0:T(8,128)(2,1)}, u32[]{:S(2)}, u32[]{:S(2)}) collective-permute-start(bf16[256,4096]{1,0:T(8,128)(2,1)} %collective-permute-done.47.refs_1_), channel_id=1, source_target_pairs={{0,1},{1,0},{2,3},{3,2},{4,5},{5,4},{6,7},{7,6}} | collective-permute-start | bytes 6291464 | tf_op jit(solution)/shard_map/ppermute | solution.py:713
  1153.2 49.8 %collective-permute-start.46 = (bf16[256,4096]{1,0:T(8,128)(2,1)}, bf16[256,4096]{1,0:T(8,128)(2,1)}, u32[]{:S(2)}, u32[]{:S(2)}) collective-permute-start(bf16[256,4096]{1,0:T(8,128)(2,1)} %add_convert_fusion.refs_7_), channel_id=1, source_target_pairs={{0,2},{1,3},{2,0},{3,1},{4,6},{5,7},{6,4},{7,5}} | collective-permute-start | bytes 6291464 | tf_op jit(solution)/shard_map/ppermute | solution.py:713
  1202.9 5.6 collective-permute-start.50
  1259.8 26.3 %collective-permute-start.51 = (bf16[128,4096]{1,0:T(8,128)(2,1)}, bf16[128,4096]{1,0:T(8,128)(2,1)}, u32[]{:S(2)}, u32[]{:S(2)}) collective-permute-start(bf16[128,4096]{1,0:T(8,128)(2,1)} %add_convert_fusion.4.refs_7_), channel_id=1, source_target_pairs={{0,2},{1,3},{2,0},{3,1},{4,6},{5,7},{6,4},{7,5}} | collective-permute-start | bytes 3145736 | tf_op jit(solution)/shard_map/ppermute | solution.py:713
  1267.7 40.0 %collective-permute-start.53 = (bf16[128,4096]{1,0:T(8,128)(2,1)}, bf16[128,4096]{1,0:T(8,128)(2,1)}, u32[]{:S(2)}, u32[]{:S(2)}) collective-permute-start(bf16[128,4096]{1,0:T(8,128)(2,1)} %add_convert_fusion.3.refs_5_), channel_id=1, source_target_pairs={{0,2},{1,3},{2,0},{3,1},{4,6},{5,7},{6,4},{7,5}} | collective-permute-start | bytes 3145736 | tf_op jit(solution)/shard_map/ppermute | solution.py:713
  (9 other events, 35.9 us)

commit v12 on v11

--- a/solution.py
+++ b/solution.py
@@ -45,21 +45,25 @@
     return lambda *refs: kernel(*refs[:n_in], *refs[n_in + n:])
 
 
-def norm_kernel(x_ref, g_ref, o_ref):
-    o_ref[...] = norm_rows(x_ref[...], g_ref[...])
-
-
-def norm_run(x_rows, gain, j, after=(), tile=128):
+def norm_kernel(x_ref, g_ref, *refs, per):
+    for k, o_ref in enumerate(refs):
+        @pl.when(lax.div(pl.program_id(0), per) == k)
+        def _():
+            o_ref[...] = norm_rows(x_ref[...], g_ref[...])
+
+
+def norm_runs(x_rows, gain, runs, after=(), tile=128):
     dim = x_rows.shape[1]
     per = RUN // tile
+    n = len(runs)
     return pl.pallas_call(
-        ordered(norm_kernel, 2, after), grid=(per,),
-        in_specs=[pl.BlockSpec((tile, dim), lambda i: (j * per + i, 0)), pl.BlockSpec((1, dim), lambda i: (0, 0))]
+        ordered(functools.partial(norm_kernel, per=per), 2, after), grid=(n * per,),
+        in_specs=[pl.BlockSpec((tile, dim), lambda i: (runs[0] * per + i, 0)), pl.BlockSpec((1, dim), lambda i: (0, 0))]
         + [ANY] * len(after),
-        out_specs=pl.BlockSpec((tile, dim), lambda i: (i, 0)),
-        out_shape=jax.ShapeDtypeStruct((RUN, dim), BF),
+        out_specs=[pl.BlockSpec((tile, dim), lambda i, k=k: (jnp.clip(i - k * per, 0, per - 1), 0)) for k in range(n)],
+        out_shape=[jax.ShapeDtypeStruct((RUN, dim), BF)] * n,
         name="norm", compiler_params=PARAMS,
-        cost_estimate=cost(RUN * dim, RUN * dim),
+        cost_estimate=cost(n * RUN * dim, n * RUN * dim),
     )(x_rows, gain, *after)
 
 
@@ -160,19 +164,22 @@
 
     q_copies = [pltpu.make_async_copy(qs[a].at[i], q_scr.at[t], q_sem.at[t]) for t, (a, i) in enumerate(q_src)]
     kv_copies = [pltpu.make_async_copy(kvs[a].at[i], kv_scr.at[r], kv_sem.at[r]) for r, (a, i) in enumerate(kv_src)]
-    first = 4
-    q_copies[0].start()
-    for cp in kv_copies[:first]:
-        cp.start()
-    for cp in q_copies[1:]:
-        cp.start()
-    for t, i in enumerate(st_src):
-        if i is not None:
+
+    def load_state(t):
+        if st_src[t] is not None:
             @pl.when(tab_ref[carried + t] != 0)
             def _():
-                pltpu.make_async_copy(sts[0].at[i], st_scr.at[t], st_sem.at[t]).start()
-    for cp in kv_copies[first:]:
+                pltpu.make_async_copy(sts[0].at[st_src[t]], st_scr.at[t], st_sem.at[t]).start()
+
+    q_copies[0].start()
+    for cp in kv_copies[:4]:
         cp.start()
+    load_state(0)
+    for cp in kv_copies[4:]:
+        cp.start()
+    for t in range(1, n_tiles):
+        q_copies[t].start()
+        load_state(t)
     kv_scr[null, 1] = jnp.zeros((256, 256), BF)
     if n_cut:
         cut_in = pltpu.make_async_copy(cut_ref.at[pl.ds(lax.axis_index('cp') * cut_scr.shape[0], cut_scr.shape[0]), :], cut_scr,
@@ -713,21 +720,22 @@
             return lax.ppermute(v, *axis_pairs)
 
         ga, gm = g_attn.reshape(1, dim), g_mlp.reshape(1, dim)
-        own = []
-        for j in range(n_run):
-            own.append(norm_run(x_rows, ga, j, after=own[-1:]))
+        own = list(norm_runs(x_rows, ga, [0]))
+        own += norm_runs(x_rows, ga, list(range(1, n_run)), after=own)
         far = [send(over_x, own[j]) for j in range(n_run)]
         mate = [send(over_core, own[j]) for j in range(n_run)]
 
         w_all = jnp.concatenate([tied(w, own[-1]).reshape(dim, -1) for w in (w_q, w_k, w_v)], axis=1)
-        tables = rope_tables(tied(run_pos, own[-1])[:, None] + jnp.arange(RUN, dtype=jnp.int32)[None, :])
+        row_pos = run_pos[:, None] + jnp.arange(RUN, dtype=jnp.int32)[None, :]
+        tables = rope_tables(tied(row_pos[:2 * n_run], own[-1]))
 
         q_here, kv_here = qkv(own + mate, w_all, (tables, 0))
         kvs, q_far = [kv_here], []
+        far_tables = rope_tables(tied(row_pos[2 * n_run:], kv_here))
 
         def far_qkv(j, after):
             here = tied(far[j], after)
-            rows = [here, send(over_core, here)], w_all, (tables, 2 * (n_run + j))
+            rows = [here, send(over_core, here)], w_all, (far_tables, 2 * j)
             if j + 1 < n_run:
                 q, kv = qkv(*rows, after=(after,))
             else:

time: 1320 us -> 1320 us (level)
  no operation moved by 1% of the time
where the time goes in v12:
time: 1320 us; the launch traced here: 1310 us
  Pallas kernels  758 us (57%)
  waiting for transfers between devices  464 us (35%)
  starting transfers between devices  39.4 us (3%)
  other arithmetic  25.3 us (2%)
  local copies, waits for them, and re-layouts  20.1 us (2%)
    ppermute x54, waiting for transfers between devices, send(): return lax.ppermute(v, *axis_pairs)  464 us
    pallas_call x5, Pallas kernels, mlp(): pl.pallas_call(ordered(functools.partial(mlp_kernel, n_in=len(bs), first=...  356 us
    pallas_call x5, Pallas kernels, flash(): pl.pallas_call(ordered(functools.partial(flash_kernel, q_src=q_src, kv_sr...  211 us
    pallas_call x6, Pallas kernels, qkv(): pl.pallas_call(ordered(functools.partial(qkv_kernel, n_in=n_in, n_q=n_q,...  97.6 us
    pallas_call x2, Pallas kernels, out_proj(): pl.pallas_call(ordered(functools.partial(out_kernel, blocks=blocks, n_w=l...  58.1 us
    ppermute x54, starting transfers between devices, send(): return lax.ppermute(v, *axis_pairs)  39.4 us
  transfers between devices with their start and end apart: 54, of which 28 were waited for; matrix products, arithmetic and copies ran while one was open for 3% of the time, Pallas kernels for 32%

profile of v12, /device:TPU:0, one launch (start us, length us, event | category | flops | bytes accessed | tf_op | source)
XLA Modules:
  0.0 1307.9 jit_solution(2368775149557383453)
XLA Ops:
  1.3 3.4 norm.2.refs_2_.refs_0_
  8.0 8.7 norm.3
  19.1 9.6 bitcast_dynamic-update-slice_fusion
  35.4 37.6 %qkv.6 = (bf16[8,1024,256]{2,1,0:T(8,128)(2,1)}, bf16[8,2,256,256]{3,2,1,0:T(8,128)(2,1)}) custom-call(bf16[256,4096]{1,0:T(8,128)(2,1)} %norm.2.refs_2_.refs_0_, bf16[256,4096]{1,0:T(8,128)(2,1)} %get-tuple-element.79.refs_1_, bf16[256,4096]{1,0:T(8,128)(2,1)} %get-tuple-element.80.refs_2_, bf16[256,4096]{1,0:T(8,128)(2,1)} %get-tuple-element.81.refs_3_, ...), custom_call_target="tpu_custom_call" | custom-call | flops 25769803776 | bytes 12582912 | tf_op jit(solution)/shard_map/qkv/pallas_call | solution.py:131
  73.8 3.4 multiply_sine_fusion
  77.5 14.1 %qkv.7 = (bf16[2,1024,256]{2,1,0:T(8,128)(2,1)}, bf16[2,2,256,256]{3,2,1,0:T(8,128)(2,1)}) custom-call(bf16[256,4096]{1,0:T(8,128)(2,1)} %collective-permute-done.5.refs_0_, bf16[256,4096]{1,0:T(8,128)(2,1)} %collective-permute-done.6.refs_1_, bf16[4096,1536]{1,0:T(8,128)(2,1)} %bitcast_dynamic-update-slice_fusion.1.refs_8_.refs_2_, ...), custom_call_target="tpu_custom_call" | custom-call | flops 6442450944 | bytes 12582912 | tf_op jit(solution)/shard_map/qkv/pallas_call | solution.py:131
  91.6 29.8 %collective-permute-done.4.refs_0_ = bf16[256,4096]{1,0:T(8,128)(2,1)} collective-permute-done((bf16[256,4096]{1,0:T(8,128)(2,1)}, bf16[256,4096]{1,0:T(8,128)(2,1)}, u32[]{:S(2)}, u32[]{:S(2)}) %collective-permute-start.4) | collective-permute-done | bytes 2097184 | tf_op jit(solution)/shard_map/ppermute | solution.py:720
  125.9 13.6 %qkv.8 = (bf16[2,1024,256]{2,1,0:T(8,128)(2,1)}, bf16[2,2,256,256]{3,2,1,0:T(8,128)(2,1)}) custom-call(bf16[256,4096]{1,0:T(8,128)(2,1)} %collective-permute-done.4.refs_0_, bf16[256,4096]{1,0:T(8,128)(2,1)} %collective-permute-done.7.refs_1_, bf16[4096,1536]{1,0:T(8,128)(2,1)} %bitcast_dynamic-update-slice_fusion.1.refs_8_.refs_2_, ...), custom_call_target="tpu_custom_call" | custom-call | flops 6442450944 | bytes 12582912 | tf_op jit(solution)/shard_map/qkv/pallas_call | solution.py:131
  139.5 50.0 %flash_part.1 = (f32[10,2,4,144,256]{4,3,2,1,0:T(8,128)}, bf16[256,4096]{1,0:T(8,128)(2,1)}, bf16[256,4096]{1,0:T(8,128)(2,1)}) custom-call(s32[845]{0:T(1024)} %dynamic-slice_reduce_fusion.refs_0_, bf16[8,1024,256]{2,1,0:T(8,128)(2,1)} %get-tuple-element.86.refs_1_, bf16[2,1024,256]{2,1,0:T(8,128)(2,1)} %get-tuple-element.94.refs_2_, ...), custom_call_target="tpu_custom_call" | custom-call | flops 38654705664 | bytes 3145728 | tf_op jit(solution)/shard_map/flash_part/pallas_call | solution.py:390
  194.7 13.8 %qkv.9 = (bf16[2,1024,256]{2,1,0:T(8,128)(2,1)}, bf16[2,2,256,256]{3,2,1,0:T(8,128)(2,1)}) custom-call(bf16[256,4096]{1,0:T(8,128)(2,1)} %collective-permute-done.8.refs_0_, bf16[256,4096]{1,0:T(8,128)(2,1)} %collective-permute-done.9.refs_1_, bf16[4096,1536]{1,0:T(8,128)(2,1)} %bitcast_dynamic-update-slice_fusion.1.refs_8_.refs_2_, ...), custom_call_target="tpu_custom_call" | custom-call | flops 6442450944 | bytes 12582912 | tf_op jit(solution)/shard_map/qkv/pallas_call | solution.py:131
  208.4 30.0 %collective-permute-done.10.refs_0_ = bf16[256,4096]{1,0:T(8,128)(2,1)} collective-permute-done((bf16[256,4096]{1,0:T(8,128)(2,1)}, bf16[256,4096]{1,0:T(8,128)(2,1)}, u32[]{:S(2)}, u32[]{:S(2)}) %collective-permute-start.10) | collective-permute-done | bytes 2097184 | tf_op jit(solution)/shard_map/ppermute | solution.py:720
  243.8 7.9 qkv.10.refs_5_.refs_7_
  253.2 10.8 qkv.11.refs_14_.refs_2_
  264.0 23.2 %collective-permute-done.12.refs_8_ = bf16[8,2,256,256]{3,2,1,0:T(8,128)(2,1)} collective-permute-done((bf16[8,2,256,256]{3,2,1,0:T(8,128)(2,1)}, bf16[8,2,256,256]{3,2,1,0:T(8,128)(2,1)}, u32[]{:S(2)}, u32[]{:S(2)}) %collective-permute-start.12) | collective-permute-done | bytes 2097184 | tf_op jit(solution)/shard_map/ppermute | solution.py:720
  287.2 11.2 collective-permute-done.13.refs_9_
  300.0 9.7 collective-permute-done.14.refs_10_
  311.3 9.7 collective-permute-done.15.refs_11_
  320.9 10.8 collective-permute-done.16.refs_12_
  331.7 29.1 %flash.4 = (bf16[2,256,1024]{2,1,0:T(8,128)(2,1)}, bf16[2,256,1024]{2,1,0:T(8,128)(2,1)}, bf16[2,256,1024]{2,1,0:T(8,128)(2,1)}, bf16[2,256,1024]{2,1,0:T(8,128)(2,1)}, f32[8,128]{1,0:T(8,128)}) custom-call(s32[845]{0:T(1024)} %dynamic-slice_reduce_fusion.refs_0_, bf16[8,1024,256]{2,1,0:T(8,128)(2,1)} %get-tuple-element.86.refs_1_, ...), custom_call_target="tpu_custom_call" | custom-call | flops 23622320128 | bytes 8388608 | tf_op jit(solution)/shard_map/flash/pallas_call | solution.py:390
  361.8 43.9 %flash.5 = (bf16[2,256,1024]{2,1,0:T(8,128)(2,1)}, bf16[2,256,1024]{2,1,0:T(8,128)(2,1)}, bf16[2,256,1024]{2,1,0:T(8,128)(2,1)}, bf16[2,256,1024]{2,1,0:T(8,128)(2,1)}, f32[8,128]{1,0:T(8,128)}) custom-call(s32[845]{0:T(1024)} %dynamic-slice_reduce_fusion.refs_0_, ...), custom_call_target="tpu_custom_call", output_to_operand_aliasing={{0}: (14, {}), {1}: (15, {}), {2}: (16, {}), {3}: (17, {})} | custom-call | flops 32212254720 | bytes 8388608 | tf_op jit(solution)/shard_map/flash/pallas_call | solution.py:390
  409.3 43.8 %flash.6 = (bf16[2,256,1024]{2,1,0:T(8,128)(2,1)}, bf16[2,256,1024]{2,1,0:T(8,128)(2,1)}, bf16[2,256,1024]{2,1,0:T(8,128)(2,1)}, bf16[2,256,1024]{2,1,0:T(8,128)(2,1)}, f32[8,128]{1,0:T(8,128)}) custom-call(s32[845]{0:T(1024)} %dynamic-slice_reduce_fusion.refs_0_, bf16[8,1024,256]{2,1,0:T(8,128)(2,1)} %get-tuple-element.86.refs_1_, ...), custom_call_target="tpu_custom_call" | custom-call | flops 32212254720 | bytes 8388608 | tf_op jit(solution)/shard_map/flash/pallas_call | solution.py:390
  456.7 3.5 collective-permute-done.25.refs_10_
  469.2 29.0 %outp.2 = (bf16[256,4096]{1,0:T(8,128)(2,1)}, bf16[256,4096]{1,0:T(8,128)(2,1)}, bf16[256,4096]{1,0:T(8,128)(2,1)}, bf16[256,4096]{1,0:T(8,128)(2,1)}) custom-call(bf16[2,256,1024]{2,1,0:T(8,128)(2,1)} %get-tuple-element.104.refs_0_, bf16[2,256,1024]{2,1,0:T(8,128)(2,1)} %collective-permute-done.17.refs_1_, ...), custom_call_target="tpu_custom_call" | custom-call | flops 17179869184 | bytes 33554432 | tf_op jit(solution)/shard_map/outp/pallas_call | solution.py:499
  498.4 7.3 collective-permute-start.29
  505.6 43.9 %flash.7 = (bf16[2,256,1024]{2,1,0:T(8,128)(2,1)}, bf16[2,256,1024]{2,1,0:T(8,128)(2,1)}, bf16[2,256,1024]{2,1,0:T(8,128)(2,1)}, bf16[2,256,1024]{2,1,0:T(8,128)(2,1)}, f32[8,128]{1,0:T(8,128)}) custom-call(s32[845]{0:T(1024)} %dynamic-slice_reduce_fusion.refs_0_, ...), custom_call_target="tpu_custom_call", output_to_operand_aliasing={{0}: (14, {}), {1}: (15, {}), {2}: (16, {}), {3}: (17, {})} | custom-call | flops 32212254720 | bytes 8388608 | tf_op jit(solution)/shard_map/flash/pallas_call | solution.py:390
  552.1 4.5 collective-permute-done.31.refs_3_
  556.6 86.7 %mlp.5 = (bf16[512,4096]{1,0:T(8,128)(2,1)}, bf16[512,4096]{1,0:T(8,128)(2,1)}) custom-call(bf16[256,4096]{1,0:T(8,128)(2,1)} %get-tuple-element.118.refs_0_, bf16[256,4096]{1,0:T(8,128)(2,1)} %collective-permute-done.29.refs_1_, bf16[256,4096]{1,0:T(8,128)(2,1)} %collective-permute-done.30.refs_2_, bf16[256,4096]{1,0:T(8,128)(2,1)} %collective-permute-done.31.refs_3_, ...), custom_call_target="tpu_custom_call" | custom-call | flops 77309411328 | bytes 75497472 | tf_op jit(solution)/shard_map/mlp/pallas_call | solution.py:584
  647.1 45.2 %collective-permute-done.37.refs_1_ = bf16[256,4096]{1,0:T(8,128)(2,1)} collective-permute-done((bf16[256,4096]{1,0:T(8,128)(2,1)}, bf16[256,4096]{1,0:T(8,128)(2,1)}, u32[]{:S(2)}, u32[]{:S(2)}) %collective-permute-start.37) | collective-permute-done | bytes 2097184 | tf_op jit(solution)/shard_map/ppermute | solution.py:720
  692.8 22.0 %collective-permute-done.34.refs_2_ = bf16[2,256,1024]{2,1,0:T(8,128)(2,1)} collective-permute-done((bf16[2,256,1024]{2,1,0:T(8,128)(2,1)}, bf16[2,256,1024]{2,1,0:T(8,128)(2,1)}, u32[]{:S(2)}, u32[]{:S(2)}) %collective-permute-start.34) | collective-permute-done | bytes 1048608 | tf_op jit(solution)/shard_map/ppermute | solution.py:720
  714.8 21.3 %collective-permute-done.35.refs_3_ = bf16[2,256,1024]{2,1,0:T(8,128)(2,1)} collective-permute-done((bf16[2,256,1024]{2,1,0:T(8,128)(2,1)}, bf16[2,256,1024]{2,1,0:T(8,128)(2,1)}, u32[]{:S(2)}, u32[]{:S(2)}) %collective-permute-start.35) | collective-permute-done | bytes 1048608 | tf_op jit(solution)/shard_map/ppermute | solution.py:720
  736.1 29.1 %outp.3 = (bf16[256,4096]{1,0:T(8,128)(2,1)}, bf16[256,4096]{1,0:T(8,128)(2,1)}, bf16[256,4096]{1,0:T(8,128)(2,1)}, bf16[256,4096]{1,0:T(8,128)(2,1)}) custom-call(bf16[2,256,1024]{2,1,0:T(8,128)(2,1)} %get-tuple-element.128.refs_0_, bf16[2,256,1024]{2,1,0:T(8,128)(2,1)} %collective-permute-done.33.refs_1_, ...), custom_call_target="tpu_custom_call" | custom-call | flops 17179869184 | bytes 33554432 | tf_op jit(solution)/shard_map/outp/pallas_call | solution.py:499
  765.2 4.3 add_convert_fusion.2.refs_7_
  769.5 86.9 %mlp.6 = (bf16[512,4096]{1,0:T(8,128)(2,1)}, bf16[512,4096]{1,0:T(8,128)(2,1)}) custom-call(bf16[256,4096]{1,0:T(8,128)(2,1)} %get-tuple-element.134.refs_0_, bf16[256,4096]{1,0:T(8,128)(2,1)} %collective-permute-done.37.refs_1_, bf16[256,4096]{1,0:T(8,128)(2,1)} %collective-permute-done.38.refs_2_, bf16[256,4096]{1,0:T(8,128)(2,1)} %collective-permute-done.39.refs_3_, ...), custom_call_target="tpu_custom_call" | custom-call | flops 77309411328 | bytes 75497472 | tf_op jit(solution)/shard_map/mlp/pallas_call | solution.py:584
  858.9 46.8 %collective-permute-done.42.refs_1_ = bf16[256,4096]{1,0:T(8,128)(2,1)} collective-permute-done((bf16[256,4096]{1,0:T(8,128)(2,1)}, bf16[256,4096]{1,0:T(8,128)(2,1)}, u32[]{:S(2)}, u32[]{:S(2)}) %collective-permute-start.42) | collective-permute-done | bytes 2097184 | tf_op jit(solution)/shard_map/ppermute | solution.py:720
  905.6 44.1 %collective-permute-done.36.refs_2_ = bf16[256,4096]{1,0:T(8,128)(2,1)} collective-permute-done((bf16[256,4096]{1,0:T(8,128)(2,1)}, bf16[256,4096]{1,0:T(8,128)(2,1)}, u32[]{:S(2)}, u32[]{:S(2)}) %collective-permute-start.36) | collective-permute-done | bytes 2097184 | tf_op jit(solution)/shard_map/ppermute | solution.py:720
  949.7 5.6 zsum.5.refs_0_
  955.3 4.4 add_convert_fusion.1.refs_7_
  959.6 86.8 %mlp.7 = (bf16[512,4096]{1,0:T(8,128)(2,1)}, bf16[512,4096]{1,0:T(8,128)(2,1)}) custom-call(bf16[256,4096]{1,0:T(8,128)(2,1)} %get-tuple-element.140.refs_0_, bf16[256,4096]{1,0:T(8,128)(2,1)} %collective-permute-done.42.refs_1_, bf16[256,4096]{1,0:T(8,128)(2,1)} %collective-permute-done.43.refs_2_, bf16[256,4096]{1,0:T(8,128)(2,1)} %collective-permute-done.44.refs_3_, ...), custom_call_target="tpu_custom_call" | custom-call | flops 77309411328 | bytes 75497472 | tf_op jit(solution)/shard_map/mlp/pallas_call | solution.py:584
  1048.5 46.8 %collective-permute-done.47.refs_1_ = bf16[256,4096]{1,0:T(8,128)(2,1)} collective-permute-done((bf16[256,4096]{1,0:T(8,128)(2,1)}, bf16[256,4096]{1,0:T(8,128)(2,1)}, u32[]{:S(2)}, u32[]{:S(2)}) %collective-permute-start.47) | collective-permute-done | bytes 2097184 | tf_op jit(solution)/shard_map/ppermute | solution.py:720
  1095.3 44.4 %collective-permute-done.41.refs_3_ = bf16[256,4096]{1,0:T(8,128)(2,1)} collective-permute-done((bf16[256,4096]{1,0:T(8,128)(2,1)}, bf16[256,4096]{1,0:T(8,128)(2,1)}, u32[]{:S(2)}, u32[]{:S(2)}) %collective-permute-start.41) | collective-permute-done | bytes 2097184 | tf_op jit(solution)/shard_map/ppermute | solution.py:720
  1139.7 5.8 zsum.6.refs_0_
  1145.5 4.3 add_convert_fusion.refs_7_
  1151.6 48.0 %mlp.8 = (bf16[256,4096]{1,0:T(8,128)(2,1)}, bf16[256,4096]{1,0:T(8,128)(2,1)}) custom-call(bf16[256,4096]{1,0:T(8,128)(2,1)} %get-tuple-element.145.refs_0_, bf16[256,4096]{1,0:T(8,128)(2,1)} %collective-permute-done.47.refs_1_, bf16[256,4096]{1,0:T(8,128)(2,1)} %collective-permute-done.48.refs_2_, bf16[256,4096]{1,0:T(8,128)(2,1)} %collective-permute-done.49.refs_3_, ...), custom_call_target="tpu_custom_call" | custom-call | flops 38654705664 | bytes 75497472 | tf_op jit(solution)/shard_map/mlp/pallas_call | solution.py:584
  1199.6 5.6 zsum.7.refs_0_
  1208.0 48.0 %mlp.9 = (bf16[256,4096]{1,0:T(8,128)(2,1)}, bf16[256,4096]{1,0:T(8,128)(2,1)}) custom-call(bf16[256,4096]{1,0:T(8,128)(2,1)} %get-tuple-element.145.refs_0_, bf16[256,4096]{1,0:T(8,128)(2,1)} %collective-permute-done.47.refs_1_, bf16[256,4096]{1,0:T(8,128)(2,1)} %collective-permute-done.48.refs_2_, bf16[256,4096]{1,0:T(8,128)(2,1)} %collective-permute-done.49.refs_3_, ...), custom_call_target="tpu_custom_call" | custom-call | flops 38654705664 | bytes 75497472 | tf_op jit(solution)/shard_map/mlp/pallas_call | solution.py:584
  1256.8 3.7 collective-permute-done.52.refs_2_
  1264.7 18.2 %collective-permute-done.51.refs_3_ = bf16[128,4096]{1,0:T(8,128)(2,1)} collective-permute-done((bf16[128,4096]{1,0:T(8,128)(2,1)}, bf16[128,4096]{1,0:T(8,128)(2,1)}, u32[]{:S(2)}, u32[]{:S(2)}) %collective-permute-start.51) | collective-permute-done | bytes 1048608 | tf_op jit(solution)/shard_map/ppermute | solution.py:720
  1286.1 18.3 %collective-permute-done.53.refs_3_ = bf16[128,4096]{1,0:T(8,128)(2,1)} collective-permute-done((bf16[128,4096]{1,0:T(8,128)(2,1)}, bf16[128,4096]{1,0:T(8,128)(2,1)}, u32[]{:S(2)}, u32[]{:S(2)}) %collective-permute-start.53) | collective-permute-done | bytes 1048608 | tf_op jit(solution)/shard_map/ppermute | solution.py:720
  (112 shorter events, 79.3 us)
Async XLA Ops:
  4.7 68.3 %collective-permute-start.5 = (bf16[256,4096]{1,0:T(8,128)(2,1)}, bf16[256,4096]{1,0:T(8,128)(2,1)}, u32[]{:S(2)}, u32[]{:S(2)}) collective-permute-start(bf16[256,4096]{1,0:T(8,128)(2,1)} %norm.2.refs_2_.refs_0_), channel_id=1, source_target_pairs={{0,2},{1,3},{2,0},{3,1},{4,6},{5,7},{6,4},{7,5}} | collective-permute-start | bytes 6291464 | tf_op jit(solution)/shard_map/ppermute | solution.py:720
  8.0 27.3 %collective-permute-start = (bf16[256,4096]{1,0:T(8,128)(2,1)}, bf16[256,4096]{1,0:T(8,128)(2,1)}, u32[]{:S(2)}, u32[]{:S(2)}) collective-permute-start(bf16[256,4096]{1,0:T(8,128)(2,1)} %norm.2.refs_2_.refs_0_), channel_id=1, source_target_pairs={{0,1},{1,0},{2,3},{3,2},{4,5},{5,4},{6,7},{7,6}} | collective-permute-start | bytes 6291464 | tf_op jit(solution)/shard_map/ppermute | solution.py:720
  16.7 18.7 %collective-permute-start.1 = (bf16[256,4096]{1,0:T(8,128)(2,1)}, bf16[256,4096]{1,0:T(8,128)(2,1)}, u32[]{:S(2)}, u32[]{:S(2)}) collective-permute-start(bf16[256,4096]{1,0:T(8,128)(2,1)} %get-tuple-element.79.refs_1_), channel_id=1, source_target_pairs={{0,1},{1,0},{2,3},{3,2},{4,5},{5,4},{6,7},{7,6}} | collective-permute-start | bytes 6291464 | tf_op jit(solution)/shard_map/ppermute | solution.py:720
  17.2 18.2 %collective-permute-start.2 = (bf16[256,4096]{1,0:T(8,128)(2,1)}, bf16[256,4096]{1,0:T(8,128)(2,1)}, u32[]{:S(2)}, u32[]{:S(2)}) collective-permute-start(bf16[256,4096]{1,0:T(8,128)(2,1)} %get-tuple-element.80.refs_2_), channel_id=1, source_target_pairs={{0,1},{1,0},{2,3},{3,2},{4,5},{5,4},{6,7},{7,6}} | collective-permute-start | bytes 6291464 | tf_op jit(solution)/shard_map/ppermute | solution.py:720
  17.2 18.2 %collective-permute-start.3 = (bf16[256,4096]{1,0:T(8,128)(2,1)}, bf16[256,4096]{1,0:T(8,128)(2,1)}, u32[]{:S(2)}, u32[]{:S(2)}) collective-permute-start(bf16[256,4096]{1,0:T(8,128)(2,1)} %get-tuple-element.81.refs_3_), channel_id=1, source_target_pairs={{0,1},{1,0},{2,3},{3,2},{4,5},{5,4},{6,7},{7,6}} | collective-permute-start | bytes 6291464 | tf_op jit(solution)/shard_map/ppermute | solution.py:720
  73.0 48.3 %collective-permute-start.4 = (bf16[256,4096]{1,0:T(8,128)(2,1)}, bf16[256,4096]{1,0:T(8,128)(2,1)}, u32[]{:S(2)}, u32[]{:S(2)}) collective-permute-start(bf16[256,4096]{1,0:T(8,128)(2,1)} %get-tuple-element.79.refs_1_), channel_id=1, source_target_pairs={{0,2},{1,3},{2,0},{3,1},{4,6},{5,7},{6,4},{7,5}} | collective-permute-start | bytes 6291464 | tf_op jit(solution)/shard_map/ppermute | solution.py:720
  121.4 68.1 %collective-permute-start.8 = (bf16[256,4096]{1,0:T(8,128)(2,1)}, bf16[256,4096]{1,0:T(8,128)(2,1)}, u32[]{:S(2)}, u32[]{:S(2)}) collective-permute-start(bf16[256,4096]{1,0:T(8,128)(2,1)} %get-tuple-element.80.refs_2_), channel_id=1, source_target_pairs={{0,2},{1,3},{2,0},{3,1},{4,6},{5,7},{6,4},{7,5}} | collective-permute-start | bytes 6291464 | tf_op jit(solution)/shard_map/ppermute | solution.py:720
  190.5 47.9 %collective-permute-start.10 = (bf16[256,4096]{1,0:T(8,128)(2,1)}, bf16[256,4096]{1,0:T(8,128)(2,1)}, u32[]{:S(2)}, u32[]{:S(2)}) collective-permute-start(bf16[256,4096]{1,0:T(8,128)(2,1)} %get-tuple-element.81.refs_3_), channel_id=1, source_target_pairs={{0,2},{1,3},{2,0},{3,1},{4,6},{5,7},{6,4},{7,5}} | collective-permute-start | bytes 6291464 | tf_op jit(solution)/shard_map/ppermute | solution.py:720
  238.4 5.4 collective-permute-start.11
  238.4 48.8 %collective-permute-start.12 = (bf16[8,2,256,256]{3,2,1,0:T(8,128)(2,1)}, bf16[8,2,256,256]{3,2,1,0:T(8,128)(2,1)}, u32[]{:S(2)}, u32[]{:S(2)}) collective-permute-start(bf16[8,2,256,256]{3,2,1,0:T(8,128)(2,1)} %get-tuple-element.87.refs_5_.refs_3_), channel_id=1, source_target_pairs={{0,4},{4,0},{1,5},{5,1},{2,6},{6,2},{3,7},{7,3}} | collective-permute-start | bytes 6291464 | tf_op jit(solution)/shard_map/ppermute | solution.py:720
  241.3 57.2 %collective-permute-start.13 = (bf16[2,2,256,256]{3,2,1,0:T(8,128)(2,1)}, bf16[2,2,256,256]{3,2,1,0:T(8,128)(2,1)}, u32[]{:S(2)}, u32[]{:S(2)}) collective-permute-start(bf16[2,2,256,256]{3,2,1,0:T(8,128)(2,1)} %get-tuple-element.90.refs_5_.refs_4_), channel_id=1, source_target_pairs={{0,4},{4,0},{1,5},{5,1},{2,6},{6,2},{3,7},{7,3}} | collective-permute-start | bytes 1572872 | tf_op jit(solution)/shard_map/ppermute | solution.py:720
  241.7 68.0 %collective-permute-start.14 = (bf16[2,2,256,256]{3,2,1,0:T(8,128)(2,1)}, bf16[2,2,256,256]{3,2,1,0:T(8,128)(2,1)}, u32[]{:S(2)}, u32[]{:S(2)}) collective-permute-start(bf16[2,2,256,256]{3,2,1,0:T(8,128)(2,1)} %get-tuple-element.93.refs_5_), channel_id=1, source_target_pairs={{0,4},{4,0},{1,5},{5,1},{2,6},{6,2},{3,7},{7,3}} | collective-permute-start | bytes 1572872 | tf_op jit(solution)/shard_map/ppermute | solution.py:720
  243.3 77.6 %collective-permute-start.15 = (bf16[2,2,256,256]{3,2,1,0:T(8,128)(2,1)}, bf16[2,2,256,256]{3,2,1,0:T(8,128)(2,1)}, u32[]{:S(2)}, u32[]{:S(2)}) collective-permute-start(bf16[2,2,256,256]{3,2,1,0:T(8,128)(2,1)} %get-tuple-element.97.refs_5_.refs_6_), channel_id=1, source_target_pairs={{0,4},{4,0},{1,5},{5,1},{2,6},{6,2},{3,7},{7,3}} | collective-permute-start | bytes 1572872 | tf_op jit(solution)/shard_map/ppermute | solution.py:720
  251.6 80.1 %collective-permute-start.16 = (bf16[2,2,256,256]{3,2,1,0:T(8,128)(2,1)}, bf16[2,2,256,256]{3,2,1,0:T(8,128)(2,1)}, u32[]{:S(2)}, u32[]{:S(2)}) collective-permute-start(bf16[2,2,256,256]{3,2,1,0:T(8,128)(2,1)} %qkv.10.refs_5_.refs_7_), channel_id=1, source_target_pairs={{0,4},{4,0},{1,5},{5,1},{2,6},{6,2},{3,7},{7,3}} | collective-permute-start | bytes 1572872 | tf_op jit(solution)/shard_map/ppermute | solution.py:720
  287.2 176.0 %collective-permute-start.20 = (bf16[1024,4096]{1,0:T(8,128)(2,1)}, bf16[1024,4096]{1,0:T(8,128)(2,1)}, u32[]{:S(2)}, u32[]{:S(2)}) collective-permute-start(bf16[1024,4096]{1,0:T(8,128)(2,1)} %bitcast.22), channel_id=1, source_target_pairs={{0,1},{1,0},{2,3},{3,2},{4,5},{5,4},{6,7},{7,6}} | collective-permute-start | bytes 25165832 | tf_op jit(solution)/shard_map/ppermute | solution.py:720
  298.5 62.4 %collective-permute-start.21 = (bf16[256,4096]{1,0:T(8,128)(2,1)}, bf16[256,4096]{1,0:T(8,128)(2,1)}, u32[]{:S(2)}, u32[]{:S(2)}) collective-permute-start(bf16[256,4096]{1,0:T(8,128)(2,1)} %get-tuple-element.109), channel_id=1, source_target_pairs={{0,2},{1,3},{2,0},{3,1},{4,6},{5,7},{6,4},{7,5}} | collective-permute-start | bytes 6291464 | tf_op jit(solution)/shard_map/ppermute | solution.py:720
  309.7 95.9 %collective-permute-start.22 = (bf16[256,4096]{1,0:T(8,128)(2,1)}, bf16[256,4096]{1,0:T(8,128)(2,1)}, u32[]{:S(2)}, u32[]{:S(2)}) collective-permute-start(bf16[256,4096]{1,0:T(8,128)(2,1)} %get-tuple-element.111), channel_id=1, source_target_pairs={{0,2},{1,3},{2,0},{3,1},{4,6},{5,7},{6,4},{7,5}} | collective-permute-start | bytes 6291464 | tf_op jit(solution)/shard_map/ppermute | solution.py:720
  360.8 47.5 %collective-permute-start.23 = (bf16[256,4096]{1,0:T(8,128)(2,1)}, bf16[256,4096]{1,0:T(8,128)(2,1)}, u32[]{:S(2)}, u32[]{:S(2)}) collective-permute-start(bf16[256,4096]{1,0:T(8,128)(2,1)} %collective-permute-done.21.refs_6_), channel_id=1, source_target_pairs={{0,4},{4,0},{1,5},{5,1},{2,6},{6,2},{3,7},{7,3}} | collective-permute-start | bytes 6291464 | tf_op jit(solution)/shard_map/ppermute | solution.py:720
  405.6 50.1 %collective-permute-start.17 = (bf16[2,256,1024]{2,1,0:T(8,128)(2,1)}, bf16[2,256,1024]{2,1,0:T(8,128)(2,1)}, u32[]{:S(2)}, u32[]{:S(2)}) collective-permute-start(bf16[2,256,1024]{2,1,0:T(8,128)(2,1)} %get-tuple-element.105), channel_id=1, source_target_pairs={{0,1},{1,0},{2,3},{3,2},{4,5},{5,4},{6,7},{7,6}} | collective-permute-start | bytes 3145736 | tf_op jit(solution)/shard_map/ppermute | solution.py:720
  405.7 50.5 %collective-permute-start.18 = (bf16[2,256,1024]{2,1,0:T(8,128)(2,1)}, bf16[2,256,1024]{2,1,0:T(8,128)(2,1)}, u32[]{:S(2)}, u32[]{:S(2)}) collective-permute-start(bf16[2,256,1024]{2,1,0:T(8,128)(2,1)} %get-tuple-element.106), channel_id=1, source_target_pairs={{0,2},{1,3},{2,0},{3,1},{4,6},{5,7},{6,4},{7,5}} | collective-permute-start | bytes 3145736 | tf_op jit(solution)/shard_map/ppermute | solution.py:720
  406.5 49.7 %collective-permute-start.19 = (bf16[2,256,1024]{2,1,0:T(8,128)(2,1)}, bf16[2,256,1024]{2,1,0:T(8,128)(2,1)}, u32[]{:S(2)}, u32[]{:S(2)}) collective-permute-start(bf16[2,256,1024]{2,1,0:T(8,128)(2,1)} %get-tuple-element.107), channel_id=1, source_target_pairs={{0,3},{1,2},{2,1},{3,0},{4,7},{5,6},{6,5},{7,4}} | collective-permute-start | bytes 3145736 | tf_op jit(solution)/shard_map/ppermute | solution.py:720
  408.4 47.3 %collective-permute-start.24 = (bf16[256,4096]{1,0:T(8,128)(2,1)}, bf16[256,4096]{1,0:T(8,128)(2,1)}, u32[]{:S(2)}, u32[]{:S(2)}) collective-permute-start(bf16[256,4096]{1,0:T(8,128)(2,1)} %collective-permute-done.22.refs_7_), channel_id=1, source_target_pairs={{0,4},{4,0},{1,5},{5,1},{2,6},{6,2},{3,7},{7,3}} | collective-permute-start | bytes 6291464 | tf_op jit(solution)/shard_map/ppermute | solution.py:720
  455.7 7.5 collective-permute-start.26
  456.2 10.0 collective-permute-start.27
  456.2 13.0 collective-permute-start.28
  498.2 53.9 %collective-permute-start.30 = (bf16[256,4096]{1,0:T(8,128)(2,1)}, bf16[256,4096]{1,0:T(8,128)(2,1)}, u32[]{:S(2)}, u32[]{:S(2)}) collective-permute-start(bf16[256,4096]{1,0:T(8,128)(2,1)} %get-tuple-element.118.refs_0_), channel_id=1, source_target_pairs={{0,1},{1,0},{2,3},{3,2},{4,5},{5,4},{6,7},{7,6}} | collective-permute-start | bytes 6291464 | tf_op jit(solution)/shard_map/ppermute | solution.py:720
  498.4 53.7 %collective-permute-start.29 = (bf16[256,4096]{1,0:T(8,128)(2,1)}, bf16[256,4096]{1,0:T(8,128)(2,1)}, u32[]{:S(2)}, u32[]{:S(2)}) collective-permute-start(bf16[256,4096]{1,0:T(8,128)(2,1)} %get-tuple-element.118.refs_0_), channel_id=1, source_target_pairs={{0,2},{1,3},{2,0},{3,1},{4,6},{5,7},{6,4},{7,5}} | collective-permute-start | bytes 6291464 | tf_op jit(solution)/shard_map/ppermute | solution.py:720
  643.3 121.8 %collective-permute-start.32 = (bf16[512,4096]{1,0:T(8,128)(2,1)}, bf16[512,4096]{1,0:T(8,128)(2,1)}, u32[]{:S(2)}, u32[]{:S(2)}) collective-permute-start(bf16[512,4096]{1,0:T(8,128)(2,1)} %get-tuple-element.127), channel_id=1, source_target_pairs={{0,1},{1,0},{2,3},{3,2},{4,5},{5,4},{6,7},{7,6}} | collective-permute-start | bytes 12582920 | tf_op jit(solution)/shard_map/ppermute | solution.py:720
  643.5 48.8 %collective-permute-start.37 = (bf16[256,4096]{1,0:T(8,128)(2,1)}, bf16[256,4096]{1,0:T(8,128)(2,1)}, u32[]{:S(2)}, u32[]{:S(2)}) collective-permute-start(bf16[256,4096]{1,0:T(8,128)(2,1)} %get-tuple-element.134.refs_0_), channel_id=1, source_target_pairs={{0,2},{1,3},{2,0},{3,1},{4,6},{5,7},{6,4},{7,5}} | collective-permute-start | bytes 6291464 | tf_op jit(solution)/shard_map/ppermute | solution.py:720
  645.2 47.1 %collective-permute-start.33 = (bf16[2,256,1024]{2,1,0:T(8,128)(2,1)}, bf16[2,256,1024]{2,1,0:T(8,128)(2,1)}, u32[]{:S(2)}, u32[]{:S(2)}) collective-permute-start(bf16[2,256,1024]{2,1,0:T(8,128)(2,1)} %get-tuple-element.129), channel_id=1, source_target_pairs={{0,1},{1,0},{2,3},{3,2},{4,5},{5,4},{6,7},{7,6}} | collective-permute-start | bytes 3145736 | tf_op jit(solution)/shard_map/ppermute | solution.py:720
  645.3 69.4 %collective-permute-start.34 = (bf16[2,256,1024]{2,1,0:T(8,128)(2,1)}, bf16[2,256,1024]{2,1,0:T(8,128)(2,1)}, u32[]{:S(2)}, u32[]{:S(2)}) collective-permute-start(bf16[2,256,1024]{2,1,0:T(8,128)(2,1)} %get-tuple-element.130), channel_id=1, source_target_pairs={{0,2},{1,3},{2,0},{3,1},{4,6},{5,7},{6,4},{7,5}} | collective-permute-start | bytes 3145736 | tf_op jit(solution)/shard_map/ppermute | solution.py:720
  645.6 90.5 %collective-permute-start.35 = (bf16[2,256,1024]{2,1,0:T(8,128)(2,1)}, bf16[2,256,1024]{2,1,0:T(8,128)(2,1)}, u32[]{:S(2)}, u32[]{:S(2)}) collective-permute-start(bf16[2,256,1024]{2,1,0:T(8,128)(2,1)} %get-tuple-element.131), channel_id=1, source_target_pairs={{0,3},{1,2},{2,1},{3,0},{4,7},{5,6},{6,5},{7,4}} | collective-permute-start | bytes 3145736 | tf_op jit(solution)/shard_map/ppermute | solution.py:720
  692.3 77.2 %collective-permute-start.38 = (bf16[256,4096]{1,0:T(8,128)(2,1)}, bf16[256,4096]{1,0:T(8,128)(2,1)}, u32[]{:S(2)}, u32[]{:S(2)}) collective-permute-start(bf16[256,4096]{1,0:T(8,128)(2,1)} %get-tuple-element.134.refs_0_), channel_id=1, source_target_pairs={{0,1},{1,0},{2,3},{3,2},{4,5},{5,4},{6,7},{7,6}} | collective-permute-start | bytes 6291464 | tf_op jit(solution)/shard_map/ppermute | solution.py:720
  692.3 77.2 %collective-permute-start.39 = (bf16[256,4096]{1,0:T(8,128)(2,1)}, bf16[256,4096]{1,0:T(8,128)(2,1)}, u32[]{:S(2)}, u32[]{:S(2)}) collective-permute-start(bf16[256,4096]{1,0:T(8,128)(2,1)} %collective-permute-done.37.refs_1_), channel_id=1, source_target_pairs={{0,1},{1,0},{2,3},{3,2},{4,5},{5,4},{6,7},{7,6}} | collective-permute-start | bytes 6291464 | tf_op jit(solution)/shard_map/ppermute | solution.py:720
  856.4 98.9 %collective-permute-start.40 = (bf16[512,4096]{1,0:T(8,128)(2,1)}, bf16[512,4096]{1,0:T(8,128)(2,1)}, u32[]{:S(2)}, u32[]{:S(2)}) collective-permute-start(bf16[512,4096]{1,0:T(8,128)(2,1)} %get-tuple-element.137), channel_id=1, source_target_pairs={{0,1},{1,0},{2,3},{3,2},{4,5},{5,4},{6,7},{7,6}} | collective-permute-start | bytes 12582920 | tf_op jit(solution)/shard_map/ppermute | solution.py:720
  856.8 48.8 %collective-permute-start.42 = (bf16[256,4096]{1,0:T(8,128)(2,1)}, bf16[256,4096]{1,0:T(8,128)(2,1)}, u32[]{:S(2)}, u32[]{:S(2)}) collective-permute-start(bf16[256,4096]{1,0:T(8,128)(2,1)} %get-tuple-element.140.refs_0_), channel_id=1, source_target_pairs={{0,2},{1,3},{2,0},{3,1},{4,6},{5,7},{6,4},{7,5}} | collective-permute-start | bytes 6291464 | tf_op jit(solution)/shard_map/ppermute | solution.py:720
  858.6 91.2 %collective-permute-start.36 = (bf16[256,4096]{1,0:T(8,128)(2,1)}, bf16[256,4096]{1,0:T(8,128)(2,1)}, u32[]{:S(2)}, u32[]{:S(2)}) collective-permute-start(bf16[256,4096]{1,0:T(8,128)(2,1)} %add_convert_fusion.2.refs_7_), channel_id=1, source_target_pairs={{0,2},{1,3},{2,0},{3,1},{4,6},{5,7},{6,4},{7,5}} | collective-permute-start | bytes 6291464 | tf_op jit(solution)/shard_map/ppermute | solution.py:720
  858.8 100.8 %collective-permute-start.43 = (bf16[256,4096]{1,0:T(8,128)(2,1)}, bf16[256,4096]{1,0:T(8,128)(2,1)}, u32[]{:S(2)}, u32[]{:S(2)}) collective-permute-start(bf16[256,4096]{1,0:T(8,128)(2,1)} %get-tuple-element.140.refs_0_), channel_id=1, source_target_pairs={{0,1},{1,0},{2,3},{3,2},{4,5},{5,4},{6,7},{7,6}} | collective-permute-start | bytes 6291464 | tf_op jit(solution)/shard_map/ppermute | solution.py:720
  905.6 54.0 %collective-permute-start.44 = (bf16[256,4096]{1,0:T(8,128)(2,1)}, bf16[256,4096]{1,0:T(8,128)(2,1)}, u32[]{:S(2)}, u32[]{:S(2)}) collective-permute-start(bf16[256,4096]{1,0:T(8,128)(2,1)} %collective-permute-done.42.refs_1_), channel_id=1, source_target_pairs={{0,1},{1,0},{2,3},{3,2},{4,5},{5,4},{6,7},{7,6}} | collective-permute-start | bytes 6291464 | tf_op jit(solution)/shard_map/ppermute | solution.py:720
  1046.4 99.1 %collective-permute-start.45 = (bf16[512,4096]{1,0:T(8,128)(2,1)}, bf16[512,4096]{1,0:T(8,128)(2,1)}, u32[]{:S(2)}, u32[]{:S(2)}) collective-permute-start(bf16[512,4096]{1,0:T(8,128)(2,1)} %get-tuple-element.143), channel_id=1, source_target_pairs={{0,1},{1,0},{2,3},{3,2},{4,5},{5,4},{6,7},{7,6}} | collective-permute-start | bytes 12582920 | tf_op jit(solution)/shard_map/ppermute | solution.py:720
  1046.5 48.8 %collective-permute-start.47 = (bf16[256,4096]{1,0:T(8,128)(2,1)}, bf16[256,4096]{1,0:T(8,128)(2,1)}, u32[]{:S(2)}, u32[]{:S(2)}) collective-permute-start(bf16[256,4096]{1,0:T(8,128)(2,1)} %get-tuple-element.145.refs_0_), channel_id=1, source_target_pairs={{0,2},{1,3},{2,0},{3,1},{4,6},{5,7},{6,4},{7,5}} | collective-permute-start | bytes 6291464 | tf_op jit(solution)/shard_map/ppermute | solution.py:720
  1048.2 91.5 %collective-permute-start.41 = (bf16[256,4096]{1,0:T(8,128)(2,1)}, bf16[256,4096]{1,0:T(8,128)(2,1)}, u32[]{:S(2)}, u32[]{:S(2)}) collective-permute-start(bf16[256,4096]{1,0:T(8,128)(2,1)} %add_convert_fusion.1.refs_7_), channel_id=1, source_target_pairs={{0,2},{1,3},{2,0},{3,1},{4,6},{5,7},{6,4},{7,5}} | collective-permute-start | bytes 6291464 | tf_op jit(solution)/shard_map/ppermute | solution.py:720
  1048.5 103.1 %collective-permute-start.48 = (bf16[256,4096]{1,0:T(8,128)(2,1)}, bf16[256,4096]{1,0:T(8,128)(2,1)}, u32[]{:S(2)}, u32[]{:S(2)}) collective-permute-start(bf16[256,4096]{1,0:T(8,128)(2,1)} %get-tuple-element.145.refs_0_), channel_id=1, source_target_pairs={{0,1},{1,0},{2,3},{3,2},{4,5},{5,4},{6,7},{7,6}} | collective-permute-start | bytes 6291464 | tf_op jit(solution)/shard_map/ppermute | solution.py:720
  1095.3 56.3 %collective-permute-start.49 = (bf16[256,4096]{1,0:T(8,128)(2,1)}, bf16[256,4096]{1,0:T(8,128)(2,1)}, u32[]{:S(2)}, u32[]{:S(2)}) collective-permute-start(bf16[256,4096]{1,0:T(8,128)(2,1)} %collective-permute-done.47.refs_1_), channel_id=1, source_target_pairs={{0,1},{1,0},{2,3},{3,2},{4,5},{5,4},{6,7},{7,6}} | collective-permute-start | bytes 6291464 | tf_op jit(solution)/shard_map/ppermute | solution.py:720
  1149.8 49.8 %collective-permute-start.46 = (bf16[256,4096]{1,0:T(8,128)(2,1)}, bf16[256,4096]{1,0:T(8,128)(2,1)}, u32[]{:S(2)}, u32[]{:S(2)}) collective-permute-start(bf16[256,4096]{1,0:T(8,128)(2,1)} %add_convert_fusion.refs_7_), channel_id=1, source_target_pairs={{0,2},{1,3},{2,0},{3,1},{4,6},{5,7},{6,4},{7,5}} | collective-permute-start | bytes 6291464 | tf_op jit(solution)/shard_map/ppermute | solution.py:720
  1199.5 5.6 collective-permute-start.50
  1256.5 26.4 %collective-permute-start.51 = (bf16[128,4096]{1,0:T(8,128)(2,1)}, bf16[128,4096]{1,0:T(8,128)(2,1)}, u32[]{:S(2)}, u32[]{:S(2)}) collective-permute-start(bf16[128,4096]{1,0:T(8,128)(2,1)} %add_convert_fusion.4.refs_7_), channel_id=1, source_target_pairs={{0,2},{1,3},{2,0},{3,1},{4,6},{5,7},{6,4},{7,5}} | collective-permute-start | bytes 3145736 | tf_op jit(solution)/shard_map/ppermute | solution.py:720
  1264.4 40.0 %collective-permute-start.53 = (bf16[128,4096]{1,0:T(8,128)(2,1)}, bf16[128,4096]{1,0:T(8,128)(2,1)}, u32[]{:S(2)}, u32[]{:S(2)}) collective-permute-start(bf16[128,4096]{1,0:T(8,128)(2,1)} %add_convert_fusion.3.refs_5_), channel_id=1, source_target_pairs={{0,2},{1,3},{2,0},{3,1},{4,6},{5,7},{6,4},{7,5}} | collective-permute-start | bytes 3145736 | tf_op jit(solution)/shard_map/ppermute | solution.py:720
  (10 other events, 54.2 us)

commit v13 on v12

--- a/solution.py
+++ b/solution.py
@@ -20,7 +20,8 @@
 ANY = pl.BlockSpec(memory_space=pltpu.HBM)
 
 
-PARAMS = pltpu.CompilerParams(vmem_limit_bytes=67043328)
+VMEM = 67043328
+PARAMS = pltpu.CompilerParams(vmem_limit_bytes=VMEM)
 
 
 def rope_tables(positions):
@@ -49,7 +50,7 @@
     for k, o_ref in enumerate(refs):
         @pl.when(lax.div(pl.program_id(0), per) == k)
         def _():
-            o_ref[...] = norm_rows(x_ref[...], g_ref[...])
+            o_ref[:] = norm_rows(x_ref[:], g_ref[:])
 
 
 def norm_runs(x_rows, gain, runs, after=(), tile=128):
@@ -94,7 +95,7 @@
         runs = [k * group + i for i in range(group)]
 
         def products():
-            return [jnp.dot(a_scr[pl.ds(pl.multiple_of(run * RUN, RUN), RUN), :], w_ref[...], preferred_element_type=F32)
+            return [jnp.dot(a_scr[pl.ds(pl.multiple_of(run * RUN, RUN), RUN), :], w_ref[:], preferred_element_type=F32)
                     for run in runs]
 
         if with_q:
@@ -297,9 +298,9 @@
 
         @pl.when((flags & (FIRST | CARRY)) == FIRST)
         def _():
-            acc_scr[...] = jnp.zeros_like(acc_scr)
-            l_scr[...] = jnp.zeros_like(l_scr)
-            m_scr[...] = jnp.full_like(m_scr, NEG)
+            acc_scr[:] = jnp.zeros_like(acc_scr)
+            l_scr[:] = jnp.zeros_like(l_scr)
+            m_scr[:] = jnp.full_like(m_scr, NEG)
 
         if n_st:
             @pl.when((flags & (FIRST | CARRY)) == (FIRST | CARRY))
@@ -457,7 +458,7 @@
         for cp in ls:
             cp.start()
     x_copy.start()
-    acc_scr[...] = jnp.zeros_like(acc_scr)
+    acc_scr[:] = jnp.zeros_like(acc_scr)
 
     def one(k, carry):
         fetch(k + n_slots - 1)
@@ -469,7 +470,7 @@
                         cp.wait()
         slot = lax.rem(k, n_slots)
         pltpu.make_async_copy(w_scr.at[slot], w_scr.at[slot], w_sem.at[slot]).wait()
-        acc_scr[...] += jnp.dot(o_scr[:, pl.ds(pl.multiple_of(k * half, half), half)], w_scr[slot], preferred_element_type=F32)
+        acc_scr[:] += jnp.dot(o_scr[:, pl.ds(pl.multiple_of(k * half, half), half)], w_scr[slot], preferred_element_type=F32)
         return carry
 
     lax.fori_loop(0, len(blocks), one, 0)
@@ -479,7 +480,7 @@
         rows = pl.ds(pl.multiple_of(r * 32, 32), 32)
         y = (x_scr[rows, :].astype(F32) + acc_scr[rows, :].astype(BF).astype(F32)).astype(BF)
         x_scr[rows, :] = y
-        o_scr[rows, :] = norm_rows(y, g_ref[...])
+        o_scr[rows, :] = norm_rows(y, g_ref[:])
         return carry
 
     stores, per = [], RUN // 32
@@ -513,8 +514,12 @@
 
 def mlp_kernel(*refs, n_in, first, rb, tn, td, nk, nd):
     b_refs = refs[:n_in]
-    wg_ref, wu_ref, wd_ref, keep_ref, send_ref, b_scr, u_scr, w_scr, d_scr, b_sem, w_sem, d_sem = refs[n_in:]
+    (wg_ref, wu_ref, wd_ref, own_ref, far_ref, b_scr, u_scr, w_scr, d_scr, keep_scr, out_scr, in_scr, b_sem, w_sem, d_sem,
+     out_sem, in_sem) = refs[n_in:]
     i = pl.program_id(0)
+    me = lax.axis_index('tp')
+    mate = {'tp': me + 1 - 2 * lax.rem(me, 2)}
+    barrier = pltpu.get_barrier_semaphore()
 
     def fetch(j):
         @pl.when(j < nk)
@@ -534,6 +539,10 @@
         up = jnp.dot(b, w_scr[slot, 1], preferred_element_type=F32)
         u_scr[rows, cols] = (jax.nn.silu(gate) * up).astype(BF)
 
+    def to_mate(n):
+        return pltpu.make_async_remote_copy(src_ref=out_scr.at[n], dst_ref=in_scr.at[n], send_sem=out_sem.at[n],
+                                            recv_sem=in_sem.at[n], device_id=mate, device_id_type=pl.DeviceIdType.MESH)
+
     @pl.when(i == 0)
     def _():
         copies = [pltpu.make_async_copy(r.at[pl.ds(first, rb), :], b_scr.at[pl.ds(k * rb, rb), :], b_sem.at[k])
@@ -542,6 +551,11 @@
         fetch(i)
         for cp in copies[1:]:
             cp.start()
+        pl.semaphore_signal(barrier, inc=1, device_id=mate, device_id_type=pl.DeviceIdType.MESH)
+
+    @pl.when(i == 1)
+    def _():
+        pl.semaphore_wait(barrier, 1)
 
     fetch(i + 1)
 
@@ -563,57 +577,82 @@
     def _():
         gated(slice(None), pl.ds(pl.multiple_of(i * tn, tn), tn), lax.rem(i, 2))
 
-    @pl.when(i >= nk)
-    def _():
-        slot = lax.rem(i - nk, 2)
+    n = i - nk
+
+    @pl.when(n > 1)
+    def _():
+        m = n - 2
+        to_mate(m).wait_recv()
+        total = (keep_scr[lax.rem(m, 2)].astype(F32) + in_scr[m].astype(F32)).astype(BF)
+        size = total.shape[0] // 2
+        own_ref[:] = total[:size]
+        far_ref[:] = total[size:]
+
+    @pl.when((n > 0) & (n <= nd))
+    def _():
+        to_mate(n - 1).start()
+
+    @pl.when((n >= 0) & (n < nd))
+    def _():
+        slot = lax.rem(n, 2)
         pltpu.make_async_copy(d_scr.at[slot], d_scr.at[slot], d_sem.at[slot]).wait()
-        d = jnp.dot(u_scr[...], d_scr[slot], preferred_element_type=F32).astype(BF)
+        d = jnp.dot(u_scr[:], d_scr[slot], preferred_element_type=F32).astype(BF)
         half = d.shape[0] // 2
-        keep_ref[...] = d[:half]
-        send_ref[...] = d[half:]
-
-
-def mlp(bs, first, rb, wg, wu, wd, after=()):
+        keep_scr[slot] = d[:half]
+        out_scr[n] = d[half:]
+
+    @pl.when(n > nd)
+    def _():
+        def sent(k, carry):
+            to_mate(k).wait_send()
+            return carry
+
+        lax.fori_loop(0, nd, sent, 0)
+
+
+def mlp(bs, first, rb, wg, wu, wd, call, after=()):
     dim = bs[0].shape[1]
     rows = rb * len(bs)
     ffn = wg.shape[1]
     td = 512
     tn = td if rows <= td else td // 2
     nk, nd = ffn // tn, dim // td
-    dn = lambda i: (0, jnp.maximum(i - nk, 0))
+    half = rows // 2
+    dn = lambda i: (0, jnp.clip(i - nk - 2, 0, nd - 1))
     return pl.pallas_call(
         ordered(functools.partial(mlp_kernel, n_in=len(bs), first=first, rb=rb, tn=tn, td=td, nk=nk, nd=nd), len(bs) + 3, after),
-        grid=(nk + nd,),
+        grid=(nk + nd + 2,),
         in_specs=[ANY] * (len(bs) + 3 + len(after)),
-        out_specs=[pl.BlockSpec((rows // 2, td), dn)] * 2,
-        out_shape=[jax.ShapeDtypeStruct((rows // 2, dim), BF)] * 2,
+        out_specs=[pl.BlockSpec((half // 2, td), dn)] * 2,
+        out_shape=[jax.ShapeDtypeStruct((half // 2, dim), BF)] * 2,
         scratch_shapes=[pltpu.VMEM((rows, dim), BF), pltpu.VMEM((rows, ffn), BF), pltpu.VMEM((2, 2, dim, tn), BF),
-                        pltpu.VMEM((2, ffn, td), BF), pltpu.SemaphoreType.DMA((len(bs),)), pltpu.SemaphoreType.DMA((2,)),
-                        pltpu.SemaphoreType.DMA((2,))],
-        name="mlp", compiler_params=PARAMS,
+                        pltpu.VMEM((2, ffn, td), BF), pltpu.VMEM((2, half, td), BF)]
+        + [pltpu.VMEM((nd, half, td), BF)] * 2 + [pltpu.SemaphoreType.DMA((n,)) for n in (len(bs), 2, 2, nd, nd)],
+        name="mlp",
+        compiler_params=pltpu.CompilerParams(vmem_limit_bytes=VMEM, collective_id=call, has_side_effects=True),
         cost_estimate=cost(6 * rows * dim * ffn, 6 * dim * ffn),
     )(*bs, wg, wu, wd, *after)
 
 
 def sum_kernel(*refs):
-    p_ref, r_ref, t_ref, y_ref, z_ref = refs[-5:]
-    total = p_ref[...].astype(F32) + r_ref[...].astype(F32) + t_ref[...].astype(F32)
-    z_ref[...] = (y_ref[...].astype(F32) + total.astype(BF).astype(F32)).astype(BF)
-
-
-def sum_rows(z, keep, recv, far, y, y_first, rows, first, total, after=(), tile=64):
-    dim = y.shape[1]
+    p_ref, t_ref, y_ref, z_ref = refs[-4:]
+    total = (p_ref[:].astype(F32) + t_ref[:].astype(F32)).astype(BF)
+    z_ref[:] = (y_ref[:].astype(F32) + total.astype(F32)).astype(BF)
+
+
+def sum_rows(z, mine, far, y, y_first, first, total, after=(), tile=64):
+    rows, dim = mine.shape
     at = lambda r0: pl.BlockSpec((tile, dim), lambda i: (r0 // tile + i, 0))
     prev = () if z is None else (z,)
     return pl.pallas_call(
-        ordered(sum_kernel, len(prev) + 4, after), grid=(rows // tile,),
-        in_specs=[ANY] * len(prev) + [at(0)] * 3 + [at(y_first)] + [ANY] * len(after),
+        ordered(sum_kernel, len(prev) + 3, after), grid=(rows // tile,),
+        in_specs=[ANY] * len(prev) + [at(0), at(0), at(y_first)] + [ANY] * len(after),
         out_specs=at(first),
         out_shape=jax.ShapeDtypeStruct((total, dim), BF),
         input_output_aliases={0: 0} if prev else {},
         name="zsum", compiler_params=PARAMS,
         cost_estimate=cost(rows * dim, 8 * rows * dim),
-    )(*prev, keep, recv, far, y, *after)
+    )(*prev, mine, far, y, *after)
 
 
 def run_positions(xi, ci, y, cps, piece):
@@ -816,25 +855,21 @@
         chunks = [(j, 0, RUN) for j in range(last)] + [(last, 0, RUN // 2), (last, RUN // 2, RUN // 2)]
 
         def finish(c):
-            j, first, size = chunks[c]
-            return sum_rows(z, *sums[c], outs[j][0], first, size, j * RUN + first, n_run * RUN,
+            j, first, _ = chunks[c]
+            return sum_rows(z, *sums[c], outs[j][0], first, j * RUN + first, n_run * RUN,
                         after=() if prev is z else (prev,))
 
         relay_b(0)
         for c, (j, first, size) in enumerate(chunks):
             b = [outs[j][1], relay[j][0], outs[j][3], relay[j][1]]
-            keep, out = mlp(b, first, size, w_gate, w_up, w_down, after=(prev,))
-            recv = send(over_core, out)
-            prev = keep
+            prev, s_far = mlp(b, first, size, w_gate, w_up, w_down, c, after=(prev,))
+            sums.append((prev, send(over_x, s_far)))
             if c < last:
                 relay_b(c + 1)
             if c == 0:
                 prev = project(1)
             elif c < n_run:
                 prev = z = finish(c - 1)
-            kept = keep if prev is keep else tied(keep, prev)
-            prev = s_far = (kept[size:].astype(F32) + recv[size:].astype(F32)).astype(BF)
-            sums.append((keep, recv, send(over_x, s_far)))
         for c in (last, n_run):
             prev = z = finish(c)
         return z[None]

time: 1320 us -> 1020 us (0.77)
  waiting for transfers between devices: 464 us -> 174 us
  other arithmetic: 25.3 us -> 7.08 us
  Pallas kernels: 758 us -> 773 us
    ppermute x54 -> x49, waiting for transfers between devices: 464 us -> 174 us  [send(): return lax.ppermute(v, *axis_pairs)]
    convert_element_type x5 -> x0, other arithmetic: 18.3 us -> none  [layer(): (kept[size:].astype(F32) + recv[size:].astype(F32)).astype(BF)]
    pallas_call x5, Pallas kernels: 356 us -> 374 us  [mlp(): pl.pallas_call(ordered(functools.partial(mlp_kernel, n_in=len(bs), first=...]
    ppermute x54 -> x49, starting transfers between devices: 39.4 us -> 39.8 us  [send(): return lax.ppermute(v, *axis_pairs)]
  transfers between devices with their start and end apart: 54 -> 49, of which waited for: 28 -> 19; matrix products, arithmetic and copies ran while one was open for 3% -> 2% of each run, Pallas kernels for 32% -> 73%
where the time goes in v13:
time: 1020 us; the launch traced here: 1010 us
  Pallas kernels  773 us (76%)
  waiting for transfers between devices  174 us (17%)
  starting transfers between devices  39.8 us (4%)
  local copies, waits for them, and re-layouts  18.8 us (2%)
    pallas_call x5, Pallas kernels, mlp(): pl.pallas_call(ordered(functools.partial(mlp_kernel, n_in=len(bs), first=...  374 us
    pallas_call x5, Pallas kernels, flash(): pl.pallas_call(ordered(functools.partial(flash_kernel, q_src=q_src, kv_sr...  211 us
    ppermute x49, waiting for transfers between devices, send(): return lax.ppermute(v, *axis_pairs)  174 us
    pallas_call x6, Pallas kernels, qkv(): pl.pallas_call(ordered(functools.partial(qkv_kernel, n_in=n_in, n_q=n_q,...  97.7 us
    pallas_call x2, Pallas kernels, out_proj(): pl.pallas_call(ordered(functools.partial(out_kernel, blocks=blocks, n_w=l...  58 us
    ppermute x49, starting transfers between devices, send(): return lax.ppermute(v, *axis_pairs)  39.8 us
    pallas_call x5, Pallas kernels, sum_rows(): pl.pallas_call(ordered(sum_kernel, len(prev) + 3, after), grid=(rows // t...  20.5 us
  transfers between devices with their start and end apart: 49, of which 19 were waited for; matrix products, arithmetic and copies ran while one was open for 2% of the time, Pallas kernels for 73%

profile of v13, /device:TPU:0, one launch (start us, length us, event | category | flops | bytes accessed | tf_op | source)
XLA Modules:
  0.0 1012.6 jit_solution(9856102895577531594)
XLA Ops:
  1.3 3.4 norm.2.refs_2_.refs_0_
  4.7 3.3 collective-permute-start.5
  8.1 8.8 norm.3
  19.2 9.5 bitcast_dynamic-update-slice_fusion
  28.8 2.8 multiply_sine_fusion.1
  33.5 2.0 bitcast_dynamic-update-slice_fusion.1.refs_8_.refs_2_
  35.6 37.7 %qkv.6 = (bf16[8,1024,256]{2,1,0:T(8,128)(2,1)}, bf16[8,2,256,256]{3,2,1,0:T(8,128)(2,1)}) custom-call(bf16[256,4096]{1,0:T(8,128)(2,1)} %norm.2.refs_2_.refs_0_, bf16[256,4096]{1,0:T(8,128)(2,1)} %get-tuple-element.75.refs_1_, bf16[256,4096]{1,0:T(8,128)(2,1)} %get-tuple-element.76.refs_2_, bf16[256,4096]{1,0:T(8,128)(2,1)} %get-tuple-element.77.refs_3_, ...), custom_call_target="tpu_custom_call" | custom-call | flops 25769803776 | bytes 12582912 | tf_op jit(solution)/shard_map/qkv/pallas_call | solution.py:132
  74.0 3.5 multiply_sine_fusion
  77.8 14.1 %qkv.7 = (bf16[2,1024,256]{2,1,0:T(8,128)(2,1)}, bf16[2,2,256,256]{3,2,1,0:T(8,128)(2,1)}) custom-call(bf16[256,4096]{1,0:T(8,128)(2,1)} %collective-permute-done.5.refs_0_, bf16[256,4096]{1,0:T(8,128)(2,1)} %collective-permute-done.6.refs_1_, bf16[4096,1536]{1,0:T(8,128)(2,1)} %bitcast_dynamic-update-slice_fusion.1.refs_8_.refs_2_, ...), custom_call_target="tpu_custom_call" | custom-call | flops 6442450944 | bytes 12582912 | tf_op jit(solution)/shard_map/qkv/pallas_call | solution.py:132
  91.9 29.8 %collective-permute-done.4.refs_0_ = bf16[256,4096]{1,0:T(8,128)(2,1)} collective-permute-done((bf16[256,4096]{1,0:T(8,128)(2,1)}, bf16[256,4096]{1,0:T(8,128)(2,1)}, u32[]{:S(2)}, u32[]{:S(2)}) %collective-permute-start.4) | collective-permute-done | bytes 2097184 | tf_op jit(solution)/shard_map/ppermute | solution.py:759
  123.3 2.9 collective-permute-done.7.refs_1_
  126.1 13.6 %qkv.8 = (bf16[2,1024,256]{2,1,0:T(8,128)(2,1)}, bf16[2,2,256,256]{3,2,1,0:T(8,128)(2,1)}) custom-call(bf16[256,4096]{1,0:T(8,128)(2,1)} %collective-permute-done.4.refs_0_, bf16[256,4096]{1,0:T(8,128)(2,1)} %collective-permute-done.7.refs_1_, bf16[4096,1536]{1,0:T(8,128)(2,1)} %bitcast_dynamic-update-slice_fusion.1.refs_8_.refs_2_, ...), custom_call_target="tpu_custom_call" | custom-call | flops 6442450944 | bytes 12582912 | tf_op jit(solution)/shard_map/qkv/pallas_call | solution.py:132
  139.8 50.1 %flash_part.1 = (f32[10,2,4,144,256]{4,3,2,1,0:T(8,128)}, bf16[256,4096]{1,0:T(8,128)(2,1)}, bf16[256,4096]{1,0:T(8,128)(2,1)}) custom-call(s32[845]{0:T(1024)} %dynamic-slice_reduce_fusion.refs_0_, bf16[8,1024,256]{2,1,0:T(8,128)(2,1)} %get-tuple-element.82.refs_1_, bf16[2,1024,256]{2,1,0:T(8,128)(2,1)} %get-tuple-element.90.refs_2_, ...), custom_call_target="tpu_custom_call" | custom-call | flops 38654705664 | bytes 3145728 | tf_op jit(solution)/shard_map/flash_part/pallas_call | solution.py:391
  192.0 3.0 collective-permute-done.9.refs_1_
  195.0 13.7 %qkv.9 = (bf16[2,1024,256]{2,1,0:T(8,128)(2,1)}, bf16[2,2,256,256]{3,2,1,0:T(8,128)(2,1)}) custom-call(bf16[256,4096]{1,0:T(8,128)(2,1)} %collective-permute-done.8.refs_0_, bf16[256,4096]{1,0:T(8,128)(2,1)} %collective-permute-done.9.refs_1_, bf16[4096,1536]{1,0:T(8,128)(2,1)} %bitcast_dynamic-update-slice_fusion.1.refs_8_.refs_2_, ...), custom_call_target="tpu_custom_call" | custom-call | flops 6442450944 | bytes 12582912 | tf_op jit(solution)/shard_map/qkv/pallas_call | solution.py:132
  208.7 30.0 %collective-permute-done.10.refs_0_ = bf16[256,4096]{1,0:T(8,128)(2,1)} collective-permute-done((bf16[256,4096]{1,0:T(8,128)(2,1)}, bf16[256,4096]{1,0:T(8,128)(2,1)}, u32[]{:S(2)}, u32[]{:S(2)}) %collective-permute-start.10) | collective-permute-done | bytes 2097184 | tf_op jit(solution)/shard_map/ppermute | solution.py:759
  244.1 7.8 qkv.10.refs_5_.refs_7_
  253.6 10.8 %qkv.11.refs_14_.refs_2_ = bf16[2,1024,256]{2,1,0:T(8,128)(2,1)} custom-call(bf16[256,4096]{1,0:T(8,128)(2,1)} %collective-permute-done.10.refs_0_, bf16[256,4096]{1,0:T(8,128)(2,1)} %collective-permute-done.11.refs_1_, bf16[4096,1536]{1,0:T(8,128)(2,1)} %bitcast_dynamic-update-slice_fusion.1.refs_8_.refs_2_, f32[8,64,256]{2,1,0:T(8,128)} %get-tuple-element.148.refs_3_, ...), custom_call_target="tpu_custom_call" | custom-call | flops 6442450944 | bytes 12582912 | tf_op jit(solution)/shard_map/qkv/pallas_call | solution.py:132
  264.4 23.2 %collective-permute-done.12.refs_8_ = bf16[8,2,256,256]{3,2,1,0:T(8,128)(2,1)} collective-permute-done((bf16[8,2,256,256]{3,2,1,0:T(8,128)(2,1)}, bf16[8,2,256,256]{3,2,1,0:T(8,128)(2,1)}, u32[]{:S(2)}, u32[]{:S(2)}) %collective-permute-start.12) | collective-permute-done | bytes 2097184 | tf_op jit(solution)/shard_map/ppermute | solution.py:759
  287.6 11.2 %collective-permute-done.13.refs_9_ = bf16[2,2,256,256]{3,2,1,0:T(8,128)(2,1)} collective-permute-done((bf16[2,2,256,256]{3,2,1,0:T(8,128)(2,1)}, bf16[2,2,256,256]{3,2,1,0:T(8,128)(2,1)}, u32[]{:S(2)}, u32[]{:S(2)}) %collective-permute-start.13) | collective-permute-done | bytes 524320 | tf_op jit(solution)/shard_map/ppermute | solution.py:759
  300.4 9.7 collective-permute-done.14.refs_10_
  311.6 9.7 collective-permute-done.15.refs_11_
  321.3 10.8 %collective-permute-done.16.refs_12_ = bf16[2,2,256,256]{3,2,1,0:T(8,128)(2,1)} collective-permute-done((bf16[2,2,256,256]{3,2,1,0:T(8,128)(2,1)}, bf16[2,2,256,256]{3,2,1,0:T(8,128)(2,1)}, u32[]{:S(2)}, u32[]{:S(2)}) %collective-permute-start.16) | collective-permute-done | bytes 524320 | tf_op jit(solution)/shard_map/ppermute | solution.py:759
  332.1 29.1 %flash.4 = (bf16[2,256,1024]{2,1,0:T(8,128)(2,1)}, bf16[2,256,1024]{2,1,0:T(8,128)(2,1)}, bf16[2,256,1024]{2,1,0:T(8,128)(2,1)}, bf16[2,256,1024]{2,1,0:T(8,128)(2,1)}, f32[8,128]{1,0:T(8,128)}) custom-call(s32[845]{0:T(1024)} %dynamic-slice_reduce_fusion.refs_0_, bf16[8,1024,256]{2,1,0:T(8,128)(2,1)} %get-tuple-element.82.refs_1_, ...), custom_call_target="tpu_custom_call" | custom-call | flops 23622320128 | bytes 8388608 | tf_op jit(solution)/shard_map/flash/pallas_call | solution.py:391
  362.1 43.9 %flash.5 = (bf16[2,256,1024]{2,1,0:T(8,128)(2,1)}, bf16[2,256,1024]{2,1,0:T(8,128)(2,1)}, bf16[2,256,1024]{2,1,0:T(8,128)(2,1)}, bf16[2,256,1024]{2,1,0:T(8,128)(2,1)}, f32[8,128]{1,0:T(8,128)}) custom-call(s32[845]{0:T(1024)} %dynamic-slice_reduce_fusion.refs_0_, ...), custom_call_target="tpu_custom_call", output_to_operand_aliasing={{0}: (14, {}), {1}: (15, {}), {2}: (16, {}), {3}: (17, {})} | custom-call | flops 32212254720 | bytes 8388608 | tf_op jit(solution)/shard_map/flash/pallas_call | solution.py:391
  409.6 43.8 %flash.6 = (bf16[2,256,1024]{2,1,0:T(8,128)(2,1)}, bf16[2,256,1024]{2,1,0:T(8,128)(2,1)}, bf16[2,256,1024]{2,1,0:T(8,128)(2,1)}, bf16[2,256,1024]{2,1,0:T(8,128)(2,1)}, f32[8,128]{1,0:T(8,128)}) custom-call(s32[845]{0:T(1024)} %dynamic-slice_reduce_fusion.refs_0_, bf16[8,1024,256]{2,1,0:T(8,128)(2,1)} %get-tuple-element.82.refs_1_, ...), custom_call_target="tpu_custom_call" | custom-call | flops 32212254720 | bytes 8388608 | tf_op jit(solution)/shard_map/flash/pallas_call | solution.py:391
  453.4 2.6 collective-permute-done.24.refs_9_
  457.1 3.5 collective-permute-done.25.refs_10_
  460.6 3.0 collective-permute-done.26.refs_11_
  463.6 3.0 collective-permute-done.27.refs_12_
  466.5 3.0 collective-permute-done.28.refs_13_
  469.5 29.0 %outp.2 = (bf16[256,4096]{1,0:T(8,128)(2,1)}, bf16[256,4096]{1,0:T(8,128)(2,1)}, bf16[256,4096]{1,0:T(8,128)(2,1)}, bf16[256,4096]{1,0:T(8,128)(2,1)}) custom-call(bf16[2,256,1024]{2,1,0:T(8,128)(2,1)} %get-tuple-element.100.refs_0_, bf16[2,256,1024]{2,1,0:T(8,128)(2,1)} %collective-permute-done.17.refs_1_, ...), custom_call_target="tpu_custom_call" | custom-call | flops 17179869184 | bytes 33554432 | tf_op jit(solution)/shard_map/outp/pallas_call | solution.py:500
  498.7 7.2 collective-permute-start.29
  506.0 43.9 %flash.7 = (bf16[2,256,1024]{2,1,0:T(8,128)(2,1)}, bf16[2,256,1024]{2,1,0:T(8,128)(2,1)}, bf16[2,256,1024]{2,1,0:T(8,128)(2,1)}, bf16[2,256,1024]{2,1,0:T(8,128)(2,1)}, f32[8,128]{1,0:T(8,128)}) custom-call(s32[845]{0:T(1024)} %dynamic-slice_reduce_fusion.refs_0_, ...), custom_call_target="tpu_custom_call", output_to_operand_aliasing={{0}: (14, {}), {1}: (15, {}), {2}: (16, {}), {3}: (17, {})} | custom-call | flops 32212254720 | bytes 8388608 | tf_op jit(solution)/shard_map/flash/pallas_call | solution.py:391
  549.8 2.6 collective-permute-done.29.refs_1_
  555.0 2.0 collective-permute-done.31.refs_3_
  558.4 91.4 %mlp.5 = (bf16[256,4096]{1,0:T(8,128)(2,1)}, bf16[256,4096]{1,0:T(8,128)(2,1)}) custom-call(bf16[256,4096]{1,0:T(8,128)(2,1)} %get-tuple-element.114.refs_0_, bf16[256,4096]{1,0:T(8,128)(2,1)} %collective-permute-done.29.refs_1_, bf16[256,4096]{1,0:T(8,128)(2,1)} %collective-permute-done.30.refs_2_, bf16[256,4096]{1,0:T(8,128)(2,1)} %collective-permute-done.31.refs_3_, ...), custom_call_target="tpu_custom_call" | custom-call | flops 77309411328 | bytes 75497472 | tf_op jit(solution)/shard_map/mlp/pallas_call | solution.py:622
  650.0 29.0 %outp.3 = (bf16[256,4096]{1,0:T(8,128)(2,1)}, bf16[256,4096]{1,0:T(8,128)(2,1)}, bf16[256,4096]{1,0:T(8,128)(2,1)}, bf16[256,4096]{1,0:T(8,128)(2,1)}) custom-call(bf16[2,256,1024]{2,1,0:T(8,128)(2,1)} %get-tuple-element.126.refs_0_, bf16[2,256,1024]{2,1,0:T(8,128)(2,1)} %collective-permute-done.36.refs_1_, ...), custom_call_target="tpu_custom_call" | custom-call | flops 17179869184 | bytes 33554432 | tf_op jit(solution)/shard_map/outp/pallas_call | solution.py:500
  681.4 91.2 %mlp.6 = (bf16[256,4096]{1,0:T(8,128)(2,1)}, bf16[256,4096]{1,0:T(8,128)(2,1)}) custom-call(bf16[256,4096]{1,0:T(8,128)(2,1)} %get-tuple-element.124.refs_0_, bf16[256,4096]{1,0:T(8,128)(2,1)} %collective-permute-done.33.refs_1_, bf16[256,4096]{1,0:T(8,128)(2,1)} %collective-permute-done.34.refs_2_, bf16[256,4096]{1,0:T(8,128)(2,1)} %collective-permute-done.35.refs_3_, ...), custom_call_target="tpu_custom_call" | custom-call | flops 77309411328 | bytes 75497472 | tf_op jit(solution)/shard_map/mlp/pallas_call | solution.py:622
  775.2 4.9 zsum.5.refs_7_.refs_0_
  780.2 90.9 %mlp.7 = (bf16[256,4096]{1,0:T(8,128)(2,1)}, bf16[256,4096]{1,0:T(8,128)(2,1)}) custom-call(bf16[256,4096]{1,0:T(8,128)(2,1)} %get-tuple-element.134.refs_0_, bf16[256,4096]{1,0:T(8,128)(2,1)} %collective-permute-done.40.refs_1_, bf16[256,4096]{1,0:T(8,128)(2,1)} %collective-permute-done.41.refs_2_, bf16[256,4096]{1,0:T(8,128)(2,1)} %collective-permute-done.42.refs_3_, ...), custom_call_target="tpu_custom_call" | custom-call | flops 77309411328 | bytes 75497472 | tf_op jit(solution)/shard_map/mlp/pallas_call | solution.py:622
  872.0 4.9 zsum.6.refs_7_.refs_0_
  877.0 50.1 %mlp.8 = (bf16[128,4096]{1,0:T(8,128)(2,1)}, bf16[128,4096]{1,0:T(8,128)(2,1)}) custom-call(bf16[256,4096]{1,0:T(8,128)(2,1)} %get-tuple-element.138.refs_0_, bf16[256,4096]{1,0:T(8,128)(2,1)} %collective-permute-done.44.refs_1_, bf16[256,4096]{1,0:T(8,128)(2,1)} %collective-permute-done.45.refs_2_, bf16[256,4096]{1,0:T(8,128)(2,1)} %collective-permute-done.46.refs_3_, ...), custom_call_target="tpu_custom_call" | custom-call | flops 38654705664 | bytes 75497472 | tf_op jit(solution)/shard_map/mlp/pallas_call | solution.py:622
  928.8 4.9 zsum.7.refs_7_.refs_0_
  933.8 50.1 %mlp.9 = (bf16[128,4096]{1,0:T(8,128)(2,1)}, bf16[128,4096]{1,0:T(8,128)(2,1)}) custom-call(bf16[256,4096]{1,0:T(8,128)(2,1)} %get-tuple-element.138.refs_0_, bf16[256,4096]{1,0:T(8,128)(2,1)} %collective-permute-done.44.refs_1_, bf16[256,4096]{1,0:T(8,128)(2,1)} %collective-permute-done.45.refs_2_, bf16[256,4096]{1,0:T(8,128)(2,1)} %collective-permute-done.46.refs_3_, ...), custom_call_target="tpu_custom_call" | custom-call | flops 38654705664 | bytes 75497472 | tf_op jit(solution)/shard_map/mlp/pallas_call | solution.py:622
  984.2 2.9 zsum.8.refs_0_
  987.1 22.5 %collective-permute-done.48.refs_2_ = bf16[128,4096]{1,0:T(8,128)(2,1)} collective-permute-done((bf16[128,4096]{1,0:T(8,128)(2,1)}, bf16[128,4096]{1,0:T(8,128)(2,1)}, u32[]{:S(2)}, u32[]{:S(2)}) %collective-permute-start.48) | collective-permute-done | bytes 1048608 | tf_op jit(solution)/shard_map/ppermute | solution.py:759
  1009.6 2.9 zsum.9
  (95 shorter events, 38.5 us)
Async XLA Ops:
  4.7 68.5 %collective-permute-start.5 = (bf16[256,4096]{1,0:T(8,128)(2,1)}, bf16[256,4096]{1,0:T(8,128)(2,1)}, u32[]{:S(2)}, u32[]{:S(2)}) collective-permute-start(bf16[256,4096]{1,0:T(8,128)(2,1)} %norm.2.refs_2_.refs_0_), channel_id=1, source_target_pairs={{0,2},{1,3},{2,0},{3,1},{4,6},{5,7},{6,4},{7,5}} | collective-permute-start | bytes 6291464 | tf_op jit(solution)/shard_map/ppermute | solution.py:759
  8.1 27.5 %collective-permute-start = (bf16[256,4096]{1,0:T(8,128)(2,1)}, bf16[256,4096]{1,0:T(8,128)(2,1)}, u32[]{:S(2)}, u32[]{:S(2)}) collective-permute-start(bf16[256,4096]{1,0:T(8,128)(2,1)} %norm.2.refs_2_.refs_0_), channel_id=1, source_target_pairs={{0,1},{1,0},{2,3},{3,2},{4,5},{5,4},{6,7},{7,6}} | collective-permute-start | bytes 6291464 | tf_op jit(solution)/shard_map/ppermute | solution.py:759
  16.8 18.8 %collective-permute-start.1 = (bf16[256,4096]{1,0:T(8,128)(2,1)}, bf16[256,4096]{1,0:T(8,128)(2,1)}, u32[]{:S(2)}, u32[]{:S(2)}) collective-permute-start(bf16[256,4096]{1,0:T(8,128)(2,1)} %get-tuple-element.75.refs_1_), channel_id=1, source_target_pairs={{0,1},{1,0},{2,3},{3,2},{4,5},{5,4},{6,7},{7,6}} | collective-permute-start | bytes 6291464 | tf_op jit(solution)/shard_map/ppermute | solution.py:759
  17.3 18.3 %collective-permute-start.2 = (bf16[256,4096]{1,0:T(8,128)(2,1)}, bf16[256,4096]{1,0:T(8,128)(2,1)}, u32[]{:S(2)}, u32[]{:S(2)}) collective-permute-start(bf16[256,4096]{1,0:T(8,128)(2,1)} %get-tuple-element.76.refs_2_), channel_id=1, source_target_pairs={{0,1},{1,0},{2,3},{3,2},{4,5},{5,4},{6,7},{7,6}} | collective-permute-start | bytes 6291464 | tf_op jit(solution)/shard_map/ppermute | solution.py:759
  17.3 18.3 %collective-permute-start.3 = (bf16[256,4096]{1,0:T(8,128)(2,1)}, bf16[256,4096]{1,0:T(8,128)(2,1)}, u32[]{:S(2)}, u32[]{:S(2)}) collective-permute-start(bf16[256,4096]{1,0:T(8,128)(2,1)} %get-tuple-element.77.refs_3_), channel_id=1, source_target_pairs={{0,1},{1,0},{2,3},{3,2},{4,5},{5,4},{6,7},{7,6}} | collective-permute-start | bytes 6291464 | tf_op jit(solution)/shard_map/ppermute | solution.py:759
  73.3 4.5 collective-permute-start.6
  73.3 48.3 %collective-permute-start.4 = (bf16[256,4096]{1,0:T(8,128)(2,1)}, bf16[256,4096]{1,0:T(8,128)(2,1)}, u32[]{:S(2)}, u32[]{:S(2)}) collective-permute-start(bf16[256,4096]{1,0:T(8,128)(2,1)} %get-tuple-element.75.refs_1_), channel_id=1, source_target_pairs={{0,2},{1,3},{2,0},{3,1},{4,6},{5,7},{6,4},{7,5}} | collective-permute-start | bytes 6291464 | tf_op jit(solution)/shard_map/ppermute | solution.py:759
  121.6 4.5 collective-permute-start.7
  121.7 68.2 %collective-permute-start.8 = (bf16[256,4096]{1,0:T(8,128)(2,1)}, bf16[256,4096]{1,0:T(8,128)(2,1)}, u32[]{:S(2)}, u32[]{:S(2)}) collective-permute-start(bf16[256,4096]{1,0:T(8,128)(2,1)} %get-tuple-element.76.refs_2_), channel_id=1, source_target_pairs={{0,2},{1,3},{2,0},{3,1},{4,6},{5,7},{6,4},{7,5}} | collective-permute-start | bytes 6291464 | tf_op jit(solution)/shard_map/ppermute | solution.py:759
  189.9 5.1 collective-permute-start.9
  190.9 47.9 %collective-permute-start.10 = (bf16[256,4096]{1,0:T(8,128)(2,1)}, bf16[256,4096]{1,0:T(8,128)(2,1)}, u32[]{:S(2)}, u32[]{:S(2)}) collective-permute-start(bf16[256,4096]{1,0:T(8,128)(2,1)} %get-tuple-element.77.refs_3_), channel_id=1, source_target_pairs={{0,2},{1,3},{2,0},{3,1},{4,6},{5,7},{6,4},{7,5}} | collective-permute-start | bytes 6291464 | tf_op jit(solution)/shard_map/ppermute | solution.py:759
  238.8 5.4 collective-permute-start.11
  238.8 48.8 %collective-permute-start.12 = (bf16[8,2,256,256]{3,2,1,0:T(8,128)(2,1)}, bf16[8,2,256,256]{3,2,1,0:T(8,128)(2,1)}, u32[]{:S(2)}, u32[]{:S(2)}) collective-permute-start(bf16[8,2,256,256]{3,2,1,0:T(8,128)(2,1)} %get-tuple-element.83.refs_5_.refs_3_), channel_id=1, source_target_pairs={{0,4},{4,0},{1,5},{5,1},{2,6},{6,2},{3,7},{7,3}} | collective-permute-start | bytes 6291464 | tf_op jit(solution)/shard_map/ppermute | solution.py:759
  241.6 57.2 %collective-permute-start.13 = (bf16[2,2,256,256]{3,2,1,0:T(8,128)(2,1)}, bf16[2,2,256,256]{3,2,1,0:T(8,128)(2,1)}, u32[]{:S(2)}, u32[]{:S(2)}) collective-permute-start(bf16[2,2,256,256]{3,2,1,0:T(8,128)(2,1)} %get-tuple-element.86.refs_5_.refs_4_), channel_id=1, source_target_pairs={{0,4},{4,0},{1,5},{5,1},{2,6},{6,2},{3,7},{7,3}} | collective-permute-start | bytes 1572872 | tf_op jit(solution)/shard_map/ppermute | solution.py:759
  242.1 68.0 %collective-permute-start.14 = (bf16[2,2,256,256]{3,2,1,0:T(8,128)(2,1)}, bf16[2,2,256,256]{3,2,1,0:T(8,128)(2,1)}, u32[]{:S(2)}, u32[]{:S(2)}) collective-permute-start(bf16[2,2,256,256]{3,2,1,0:T(8,128)(2,1)} %get-tuple-element.89.refs_5_), channel_id=1, source_target_pairs={{0,4},{4,0},{1,5},{5,1},{2,6},{6,2},{3,7},{7,3}} | collective-permute-start | bytes 1572872 | tf_op jit(solution)/shard_map/ppermute | solution.py:759
  243.7 77.6 %collective-permute-start.15 = (bf16[2,2,256,256]{3,2,1,0:T(8,128)(2,1)}, bf16[2,2,256,256]{3,2,1,0:T(8,128)(2,1)}, u32[]{:S(2)}, u32[]{:S(2)}) collective-permute-start(bf16[2,2,256,256]{3,2,1,0:T(8,128)(2,1)} %get-tuple-element.93.refs_5_.refs_6_), channel_id=1, source_target_pairs={{0,4},{4,0},{1,5},{5,1},{2,6},{6,2},{3,7},{7,3}} | collective-permute-start | bytes 1572872 | tf_op jit(solution)/shard_map/ppermute | solution.py:759
  252.0 80.1 %collective-permute-start.16 = (bf16[2,2,256,256]{3,2,1,0:T(8,128)(2,1)}, bf16[2,2,256,256]{3,2,1,0:T(8,128)(2,1)}, u32[]{:S(2)}, u32[]{:S(2)}) collective-permute-start(bf16[2,2,256,256]{3,2,1,0:T(8,128)(2,1)} %qkv.10.refs_5_.refs_7_), channel_id=1, source_target_pairs={{0,4},{4,0},{1,5},{5,1},{2,6},{6,2},{3,7},{7,3}} | collective-permute-start | bytes 1572872 | tf_op jit(solution)/shard_map/ppermute | solution.py:759
  287.6 176.0 %collective-permute-start.20 = (bf16[1024,4096]{1,0:T(8,128)(2,1)}, bf16[1024,4096]{1,0:T(8,128)(2,1)}, u32[]{:S(2)}, u32[]{:S(2)}) collective-permute-start(bf16[1024,4096]{1,0:T(8,128)(2,1)} %bitcast.22), channel_id=1, source_target_pairs={{0,1},{1,0},{2,3},{3,2},{4,5},{5,4},{6,7},{7,6}} | collective-permute-start | bytes 25165832 | tf_op jit(solution)/shard_map/ppermute | solution.py:759
  298.8 62.4 %collective-permute-start.21 = (bf16[256,4096]{1,0:T(8,128)(2,1)}, bf16[256,4096]{1,0:T(8,128)(2,1)}, u32[]{:S(2)}, u32[]{:S(2)}) collective-permute-start(bf16[256,4096]{1,0:T(8,128)(2,1)} %get-tuple-element.105), channel_id=1, source_target_pairs={{0,2},{1,3},{2,0},{3,1},{4,6},{5,7},{6,4},{7,5}} | collective-permute-start | bytes 6291464 | tf_op jit(solution)/shard_map/ppermute | solution.py:759
  310.0 95.9 %collective-permute-start.22 = (bf16[256,4096]{1,0:T(8,128)(2,1)}, bf16[256,4096]{1,0:T(8,128)(2,1)}, u32[]{:S(2)}, u32[]{:S(2)}) collective-permute-start(bf16[256,4096]{1,0:T(8,128)(2,1)} %get-tuple-element.107), channel_id=1, source_target_pairs={{0,2},{1,3},{2,0},{3,1},{4,6},{5,7},{6,4},{7,5}} | collective-permute-start | bytes 6291464 | tf_op jit(solution)/shard_map/ppermute | solution.py:759
  361.2 47.5 %collective-permute-start.23 = (bf16[256,4096]{1,0:T(8,128)(2,1)}, bf16[256,4096]{1,0:T(8,128)(2,1)}, u32[]{:S(2)}, u32[]{:S(2)}) collective-permute-start(bf16[256,4096]{1,0:T(8,128)(2,1)} %collective-permute-done.21.refs_6_), channel_id=1, source_target_pairs={{0,4},{4,0},{1,5},{5,1},{2,6},{6,2},{3,7},{7,3}} | collective-permute-start | bytes 6291464 | tf_op jit(solution)/shard_map/ppermute | solution.py:759
  406.0 50.1 %collective-permute-start.17 = (bf16[2,256,1024]{2,1,0:T(8,128)(2,1)}, bf16[2,256,1024]{2,1,0:T(8,128)(2,1)}, u32[]{:S(2)}, u32[]{:S(2)}) collective-permute-start(bf16[2,256,1024]{2,1,0:T(8,128)(2,1)} %get-tuple-element.101), channel_id=1, source_target_pairs={{0,1},{1,0},{2,3},{3,2},{4,5},{5,4},{6,7},{7,6}} | collective-permute-start | bytes 3145736 | tf_op jit(solution)/shard_map/ppermute | solution.py:759
  406.0 50.5 %collective-permute-start.18 = (bf16[2,256,1024]{2,1,0:T(8,128)(2,1)}, bf16[2,256,1024]{2,1,0:T(8,128)(2,1)}, u32[]{:S(2)}, u32[]{:S(2)}) collective-permute-start(bf16[2,256,1024]{2,1,0:T(8,128)(2,1)} %get-tuple-element.102), channel_id=1, source_target_pairs={{0,2},{1,3},{2,0},{3,1},{4,6},{5,7},{6,4},{7,5}} | collective-permute-start | bytes 3145736 | tf_op jit(solution)/shard_map/ppermute | solution.py:759
  406.9 49.7 %collective-permute-start.19 = (bf16[2,256,1024]{2,1,0:T(8,128)(2,1)}, bf16[2,256,1024]{2,1,0:T(8,128)(2,1)}, u32[]{:S(2)}, u32[]{:S(2)}) collective-permute-start(bf16[2,256,1024]{2,1,0:T(8,128)(2,1)} %get-tuple-element.103), channel_id=1, source_target_pairs={{0,3},{1,2},{2,1},{3,0},{4,7},{5,6},{6,5},{7,4}} | collective-permute-start | bytes 3145736 | tf_op jit(solution)/shard_map/ppermute | solution.py:759
  408.7 47.4 %collective-permute-start.24 = (bf16[256,4096]{1,0:T(8,128)(2,1)}, bf16[256,4096]{1,0:T(8,128)(2,1)}, u32[]{:S(2)}, u32[]{:S(2)}) collective-permute-start(bf16[256,4096]{1,0:T(8,128)(2,1)} %collective-permute-done.22.refs_7_), channel_id=1, source_target_pairs={{0,4},{4,0},{1,5},{5,1},{2,6},{6,2},{3,7},{7,3}} | collective-permute-start | bytes 6291464 | tf_op jit(solution)/shard_map/ppermute | solution.py:759
  456.0 4.5 collective-permute-start.25
  456.1 7.5 collective-permute-start.26
  456.6 10.0 collective-permute-start.27
  456.6 13.0 %collective-permute-start.28 = (bf16[256,4096]{1,0:T(8,128)(2,1)}, bf16[256,4096]{1,0:T(8,128)(2,1)}, u32[]{:S(2)}, u32[]{:S(2)}) collective-permute-start(bf16[256,4096]{1,0:T(8,128)(2,1)} %collective-permute-done.24.refs_9_), channel_id=1, source_target_pairs={{0,1},{1,0},{2,3},{3,2},{4,5},{5,4},{6,7},{7,6}} | collective-permute-start | bytes 6291464 | tf_op jit(solution)/shard_map/ppermute | solution.py:759
  498.6 56.1 %collective-permute-start.30 = (bf16[256,4096]{1,0:T(8,128)(2,1)}, bf16[256,4096]{1,0:T(8,128)(2,1)}, u32[]{:S(2)}, u32[]{:S(2)}) collective-permute-start(bf16[256,4096]{1,0:T(8,128)(2,1)} %get-tuple-element.114.refs_0_), channel_id=1, source_target_pairs={{0,1},{1,0},{2,3},{3,2},{4,5},{5,4},{6,7},{7,6}} | collective-permute-start | bytes 6291464 | tf_op jit(solution)/shard_map/ppermute | solution.py:759
  498.7 53.7 %collective-permute-start.29 = (bf16[256,4096]{1,0:T(8,128)(2,1)}, bf16[256,4096]{1,0:T(8,128)(2,1)}, u32[]{:S(2)}, u32[]{:S(2)}) collective-permute-start(bf16[256,4096]{1,0:T(8,128)(2,1)} %get-tuple-element.114.refs_0_), channel_id=1, source_target_pairs={{0,2},{1,3},{2,0},{3,1},{4,6},{5,7},{6,4},{7,5}} | collective-permute-start | bytes 6291464 | tf_op jit(solution)/shard_map/ppermute | solution.py:759
  552.4 129.0 %collective-permute-start.34 = (bf16[256,4096]{1,0:T(8,128)(2,1)}, bf16[256,4096]{1,0:T(8,128)(2,1)}, u32[]{:S(2)}, u32[]{:S(2)}) collective-permute-start(bf16[256,4096]{1,0:T(8,128)(2,1)} %get-tuple-element.124.refs_0_), channel_id=1, source_target_pairs={{0,1},{1,0},{2,3},{3,2},{4,5},{5,4},{6,7},{7,6}} | collective-permute-start | bytes 6291464 | tf_op jit(solution)/shard_map/ppermute | solution.py:759
  553.0 96.9 %collective-permute-start.33 = (bf16[256,4096]{1,0:T(8,128)(2,1)}, bf16[256,4096]{1,0:T(8,128)(2,1)}, u32[]{:S(2)}, u32[]{:S(2)}) collective-permute-start(bf16[256,4096]{1,0:T(8,128)(2,1)} %get-tuple-element.124.refs_0_), channel_id=1, source_target_pairs={{0,2},{1,3},{2,0},{3,1},{4,6},{5,7},{6,4},{7,5}} | collective-permute-start | bytes 6291464 | tf_op jit(solution)/shard_map/ppermute | solution.py:759
  554.7 95.3 %collective-permute-start.36 = (bf16[2,256,1024]{2,1,0:T(8,128)(2,1)}, bf16[2,256,1024]{2,1,0:T(8,128)(2,1)}, u32[]{:S(2)}, u32[]{:S(2)}) collective-permute-start(bf16[2,256,1024]{2,1,0:T(8,128)(2,1)} %get-tuple-element.127), channel_id=1, source_target_pairs={{0,1},{1,0},{2,3},{3,2},{4,5},{5,4},{6,7},{7,6}} | collective-permute-start | bytes 3145736 | tf_op jit(solution)/shard_map/ppermute | solution.py:759
  554.7 95.3 %collective-permute-start.37 = (bf16[2,256,1024]{2,1,0:T(8,128)(2,1)}, bf16[2,256,1024]{2,1,0:T(8,128)(2,1)}, u32[]{:S(2)}, u32[]{:S(2)}) collective-permute-start(bf16[2,256,1024]{2,1,0:T(8,128)(2,1)} %get-tuple-element.128), channel_id=1, source_target_pairs={{0,2},{1,3},{2,0},{3,1},{4,6},{5,7},{6,4},{7,5}} | collective-permute-start | bytes 3145736 | tf_op jit(solution)/shard_map/ppermute | solution.py:759
  556.9 93.0 %collective-permute-start.38 = (bf16[2,256,1024]{2,1,0:T(8,128)(2,1)}, bf16[2,256,1024]{2,1,0:T(8,128)(2,1)}, u32[]{:S(2)}, u32[]{:S(2)}) collective-permute-start(bf16[2,256,1024]{2,1,0:T(8,128)(2,1)} %get-tuple-element.129), channel_id=1, source_target_pairs={{0,3},{1,2},{2,1},{3,0},{4,7},{5,6},{6,5},{7,4}} | collective-permute-start | bytes 3145736 | tf_op jit(solution)/shard_map/ppermute | solution.py:759
  649.8 31.6 %collective-permute-start.35 = (bf16[256,4096]{1,0:T(8,128)(2,1)}, bf16[256,4096]{1,0:T(8,128)(2,1)}, u32[]{:S(2)}, u32[]{:S(2)}) collective-permute-start(bf16[256,4096]{1,0:T(8,128)(2,1)} %collective-permute-done.33.refs_1_), channel_id=1, source_target_pairs={{0,1},{1,0},{2,3},{3,2},{4,5},{5,4},{6,7},{7,6}} | collective-permute-start | bytes 6291464 | tf_op jit(solution)/shard_map/ppermute | solution.py:759
  679.0 101.2 %collective-permute-start.41 = (bf16[256,4096]{1,0:T(8,128)(2,1)}, bf16[256,4096]{1,0:T(8,128)(2,1)}, u32[]{:S(2)}, u32[]{:S(2)}) collective-permute-start(bf16[256,4096]{1,0:T(8,128)(2,1)} %get-tuple-element.134.refs_0_), channel_id=1, source_target_pairs={{0,1},{1,0},{2,3},{3,2},{4,5},{5,4},{6,7},{7,6}} | collective-permute-start | bytes 6291464 | tf_op jit(solution)/shard_map/ppermute | solution.py:759
  679.4 93.2 %collective-permute-start.40 = (bf16[256,4096]{1,0:T(8,128)(2,1)}, bf16[256,4096]{1,0:T(8,128)(2,1)}, u32[]{:S(2)}, u32[]{:S(2)}) collective-permute-start(bf16[256,4096]{1,0:T(8,128)(2,1)} %get-tuple-element.134.refs_0_), channel_id=1, source_target_pairs={{0,2},{1,3},{2,0},{3,1},{4,6},{5,7},{6,4},{7,5}} | collective-permute-start | bytes 6291464 | tf_op jit(solution)/shard_map/ppermute | solution.py:759
  679.7 93.8 %collective-permute-start.32 = (bf16[256,4096]{1,0:T(8,128)(2,1)}, bf16[256,4096]{1,0:T(8,128)(2,1)}, u32[]{:S(2)}, u32[]{:S(2)}) collective-permute-start(bf16[256,4096]{1,0:T(8,128)(2,1)} %get-tuple-element.123), channel_id=1, source_target_pairs={{0,2},{1,3},{2,0},{3,1},{4,6},{5,7},{6,4},{7,5}} | collective-permute-start | bytes 6291464 | tf_op jit(solution)/shard_map/ppermute | solution.py:759
  772.6 7.6 collective-permute-start.42
  773.2 103.8 %collective-permute-start.45 = (bf16[256,4096]{1,0:T(8,128)(2,1)}, bf16[256,4096]{1,0:T(8,128)(2,1)}, u32[]{:S(2)}, u32[]{:S(2)}) collective-permute-start(bf16[256,4096]{1,0:T(8,128)(2,1)} %get-tuple-element.138.refs_0_), channel_id=1, source_target_pairs={{0,1},{1,0},{2,3},{3,2},{4,5},{5,4},{6,7},{7,6}} | collective-permute-start | bytes 6291464 | tf_op jit(solution)/shard_map/ppermute | solution.py:759
  773.2 97.9 %collective-permute-start.44 = (bf16[256,4096]{1,0:T(8,128)(2,1)}, bf16[256,4096]{1,0:T(8,128)(2,1)}, u32[]{:S(2)}, u32[]{:S(2)}) collective-permute-start(bf16[256,4096]{1,0:T(8,128)(2,1)} %get-tuple-element.138.refs_0_), channel_id=1, source_target_pairs={{0,2},{1,3},{2,0},{3,1},{4,6},{5,7},{6,4},{7,5}} | collective-permute-start | bytes 6291464 | tf_op jit(solution)/shard_map/ppermute | solution.py:759
  773.5 98.5 %collective-permute-start.39 = (bf16[256,4096]{1,0:T(8,128)(2,1)}, bf16[256,4096]{1,0:T(8,128)(2,1)}, u32[]{:S(2)}, u32[]{:S(2)}) collective-permute-start(bf16[256,4096]{1,0:T(8,128)(2,1)} %get-tuple-element.132), channel_id=1, source_target_pairs={{0,2},{1,3},{2,0},{3,1},{4,6},{5,7},{6,4},{7,5}} | collective-permute-start | bytes 6291464 | tf_op jit(solution)/shard_map/ppermute | solution.py:759
  871.1 5.8 collective-permute-start.46
  871.7 57.1 %collective-permute-start.43 = (bf16[256,4096]{1,0:T(8,128)(2,1)}, bf16[256,4096]{1,0:T(8,128)(2,1)}, u32[]{:S(2)}, u32[]{:S(2)}) collective-permute-start(bf16[256,4096]{1,0:T(8,128)(2,1)} %get-tuple-element.137), channel_id=1, source_target_pairs={{0,2},{1,3},{2,0},{3,1},{4,6},{5,7},{6,4},{7,5}} | collective-permute-start | bytes 6291464 | tf_op jit(solution)/shard_map/ppermute | solution.py:759
  927.1 57.1 %collective-permute-start.47 = (bf16[128,4096]{1,0:T(8,128)(2,1)}, bf16[128,4096]{1,0:T(8,128)(2,1)}, u32[]{:S(2)}, u32[]{:S(2)}) collective-permute-start(bf16[128,4096]{1,0:T(8,128)(2,1)} %get-tuple-element.141), channel_id=1, source_target_pairs={{0,2},{1,3},{2,0},{3,1},{4,6},{5,7},{6,4},{7,5}} | collective-permute-start | bytes 3145736 | tf_op jit(solution)/shard_map/ppermute | solution.py:759
  983.9 25.7 %collective-permute-start.48 = (bf16[128,4096]{1,0:T(8,128)(2,1)}, bf16[128,4096]{1,0:T(8,128)(2,1)}, u32[]{:S(2)}, u32[]{:S(2)}) collective-permute-start(bf16[128,4096]{1,0:T(8,128)(2,1)} %get-tuple-element.144), channel_id=1, source_target_pairs={{0,2},{1,3},{2,0},{3,1},{4,6},{5,7},{6,4},{7,5}} | collective-permute-start | bytes 3145736 | tf_op jit(solution)/shard_map/ppermute | solution.py:759
  (4 other events, 29.7 us)

commit v14 on v13

--- a/solution.py
+++ b/solution.py
@@ -181,7 +181,7 @@
     for t in range(1, n_tiles):
         q_copies[t].start()
         load_state(t)
-    kv_scr[null, 1] = jnp.zeros((256, 256), BF)
+    kv_scr[null, 1] = jnp.zeros((RUN, RUN), BF)
     if n_cut:
         cut_in = pltpu.make_async_copy(cut_ref.at[pl.ds(lax.axis_index('cp') * cut_scr.shape[0], cut_scr.shape[0]), :], cut_scr,
                                        cut_sem)
@@ -398,7 +398,7 @@
             in_specs=[ANY] * (n_in - 1 + len(after)),
             out_specs=[ANY] * len(out_shape),
             scratch_shapes=[pltpu.VMEM((n_tiles, nq, RUN), BF),
-                            pltpu.VMEM((n_runs + 1, 2, 256, 256), BF),
+                            pltpu.VMEM((n_runs + 1, 2, RUN, RUN), BF),
                             pltpu.VMEM((n_tiles if final else 1, RUN, nq), BF),
                             pltpu.VMEM((n_tiles if has_st else 1, *state), F32),
                             pltpu.VMEM((G, 4 * RUN, RUN), F32),
@@ -476,16 +476,18 @@
     lax.fori_loop(0, len(blocks), one, 0)
     x_copy.wait()
 
-    def rows32(r, carry):
-        rows = pl.ds(pl.multiple_of(r * 32, 32), 32)
+    strip = 32
+
+    def one_strip(r, carry):
+        rows = pl.ds(pl.multiple_of(r * strip, strip), strip)
         y = (x_scr[rows, :].astype(F32) + acc_scr[rows, :].astype(BF).astype(F32)).astype(BF)
         x_scr[rows, :] = y
         o_scr[rows, :] = norm_rows(y, g_ref[:])
         return carry
 
-    stores, per = [], RUN // 32
+    stores, per = [], RUN // strip
     for i in range(n_run):
-        lax.fori_loop(i * per, (i + 1) * per, rows32, 0)
+        lax.fori_loop(i * per, (i + 1) * per, one_strip, 0)
         for k, scr in enumerate((x_scr, o_scr)):
             stores.append(pltpu.make_async_copy(scr.at[pl.ds(i * RUN, RUN), :], outs[2 * i + k], out_sem.at[2 * i + k]))
             stores[-1].start()
@@ -512,13 +514,19 @@
     )(*os, *ws, x_rows, gain, *after)
 
 
-def mlp_kernel(*refs, n_in, first, rb, tn, td, nk, nd):
+def mlp_kernel(*refs, n_in, first, rb, tn, td, nk, nd, cross):
     b_refs = refs[:n_in]
-    (wg_ref, wu_ref, wd_ref, own_ref, far_ref, b_scr, u_scr, w_scr, d_scr, keep_scr, out_scr, in_scr, b_sem, w_sem, d_sem,
-     out_sem, in_sem) = refs[n_in:]
+    wg_ref, wu_ref, wd_ref, *outs = refs[n_in:n_in + (4 if cross else 5)]
+    (b_scr, u_scr, w_scr, d_scr, keep_scr, out_scr, in_scr, b_sem, w_sem, d_sem, out_sem, in_sem,
+     *more) = refs[n_in + (4 if cross else 5):]
     i = pl.program_id(0)
     me = lax.axis_index('tp')
     mate = {'tp': me + 1 - 2 * lax.rem(me, 2)}
+    peers = [mate]
+    if cross:
+        own_scr, far_scr, back_scr, far_sem, back_sem = more
+        half_tp = lax.axis_size('tp') // 2
+        peers.append({'tp': lax.rem(me + half_tp, 2 * half_tp)})
     barrier = pltpu.get_barrier_semaphore()
 
     def fetch(j):
@@ -542,6 +550,10 @@
     def to_mate(n):
         return pltpu.make_async_remote_copy(src_ref=out_scr.at[n], dst_ref=in_scr.at[n], send_sem=out_sem.at[n],
                                             recv_sem=in_sem.at[n], device_id=mate, device_id_type=pl.DeviceIdType.MESH)
+
+    def to_far(n):
+        return pltpu.make_async_remote_copy(src_ref=far_scr.at[n], dst_ref=back_scr.at[n], send_sem=far_sem.at[n],
+                                            recv_sem=back_sem.at[n], device_id=peers[-1], device_id_type=pl.DeviceIdType.MESH)
 
     @pl.when(i == 0)
     def _():
@@ -551,17 +563,19 @@
         fetch(i)
         for cp in copies[1:]:
             cp.start()
-        pl.semaphore_signal(barrier, inc=1, device_id=mate, device_id_type=pl.DeviceIdType.MESH)
+        for peer in peers:
+            pl.semaphore_signal(barrier, inc=1, device_id=peer, device_id_type=pl.DeviceIdType.MESH)
 
     @pl.when(i == 1)
     def _():
-        pl.semaphore_wait(barrier, 1)
+        pl.semaphore_wait(barrier, len(peers))
 
     fetch(i + 1)
 
     @pl.when(i < nk)
     def _():
-        pltpu.make_async_copy(w_scr.at[lax.rem(i, 2)], w_scr.at[lax.rem(i, 2)], w_sem.at[lax.rem(i, 2)]).wait()
+        slot = lax.rem(i, 2)
+        pltpu.make_async_copy(w_scr.at[slot], w_scr.at[slot], w_sem.at[slot]).wait()
 
     @pl.when(i == 0)
     def _():
@@ -579,18 +593,14 @@
 
     n = i - nk
 
-    @pl.when(n > 1)
-    def _():
-        m = n - 2
-        to_mate(m).wait_recv()
-        total = (keep_scr[lax.rem(m, 2)].astype(F32) + in_scr[m].astype(F32)).astype(BF)
-        size = total.shape[0] // 2
-        own_ref[:] = total[:size]
-        far_ref[:] = total[size:]
-
     @pl.when((n > 0) & (n <= nd))
     def _():
         to_mate(n - 1).start()
+
+    if cross:
+        @pl.when((n > 1) & (n <= nd + 1))
+        def _():
+            to_far(n - 2).start()
 
     @pl.when((n >= 0) & (n < nd))
     def _():
@@ -601,16 +611,38 @@
         keep_scr[slot] = d[:half]
         out_scr[n] = d[half:]
 
-    @pl.when(n > nd)
+    @pl.when((n > 0) & (n <= nd))
+    def _():
+        m = n - 1
+        to_mate(m).wait_recv()
+        total = (keep_scr[lax.rem(m, 2)].astype(F32) + in_scr[m].astype(F32)).astype(BF)
+        size = total.shape[0] // 2
+        if cross:
+            own_scr[m] = total[:size]
+            far_scr[m] = total[size:]
+        else:
+            outs[0][:] = total[:size]
+            outs[1][:] = total[size:]
+
+    if cross:
+        @pl.when(n > nd)
+        def _():
+            m = n - nd - 1
+            to_far(m).wait_recv()
+            outs[0][:] = (own_scr[m].astype(F32) + back_scr[m].astype(F32)).astype(BF)
+
+    @pl.when(i == pl.num_programs(0) - 1)
     def _():
         def sent(k, carry):
             to_mate(k).wait_send()
+            if cross:
+                to_far(k).wait_send()
             return carry
 
         lax.fori_loop(0, nd, sent, 0)
 
 
-def mlp(bs, first, rb, wg, wu, wd, call, after=()):
+def mlp(bs, first, rb, wg, wu, wd, call, cross=False, after=()):
     dim = bs[0].shape[1]
     rows = rb * len(bs)
     ffn = wg.shape[1]
@@ -618,41 +650,47 @@
     tn = td if rows <= td else td // 2
     nk, nd = ffn // tn, dim // td
     half = rows // 2
-    dn = lambda i: (0, jnp.clip(i - nk - 2, 0, nd - 1))
+    lag = nk + 1 + nd * cross
+    n_out = 1 if cross else 2
+    tiles = pltpu.VMEM((nd, half, td), BF)
+    sem = pltpu.SemaphoreType.DMA
     return pl.pallas_call(
-        ordered(functools.partial(mlp_kernel, n_in=len(bs), first=first, rb=rb, tn=tn, td=td, nk=nk, nd=nd), len(bs) + 3, after),
-        grid=(nk + nd + 2,),
+        ordered(functools.partial(mlp_kernel, n_in=len(bs), first=first, rb=rb, tn=tn, td=td, nk=nk, nd=nd, cross=cross),
+                len(bs) + 3, after),
+        grid=(nd + lag,),
         in_specs=[ANY] * (len(bs) + 3 + len(after)),
-        out_specs=[pl.BlockSpec((half // 2, td), dn)] * 2,
-        out_shape=[jax.ShapeDtypeStruct((half // 2, dim), BF)] * 2,
+        out_specs=[pl.BlockSpec((rb, td), lambda i: (0, jnp.clip(i - lag, 0, nd - 1)))] * n_out,
+        out_shape=[jax.ShapeDtypeStruct((rb, dim), BF)] * n_out,
         scratch_shapes=[pltpu.VMEM((rows, dim), BF), pltpu.VMEM((rows, ffn), BF), pltpu.VMEM((2, 2, dim, tn), BF),
-                        pltpu.VMEM((2, ffn, td), BF), pltpu.VMEM((2, half, td), BF)]
-        + [pltpu.VMEM((nd, half, td), BF)] * 2 + [pltpu.SemaphoreType.DMA((n,)) for n in (len(bs), 2, 2, nd, nd)],
+                        pltpu.VMEM((2, ffn, td), BF), pltpu.VMEM((2, half, td), BF), tiles, tiles]
+        + [sem((n,)) for n in (len(bs), 2, 2, nd, nd)]
+        + ([pltpu.VMEM((nd, rb, td), BF)] * 3 + [sem((nd,))] * 2 if cross else []),
         name="mlp",
         compiler_params=pltpu.CompilerParams(vmem_limit_bytes=VMEM, collective_id=call, has_side_effects=True),
         cost_estimate=cost(6 * rows * dim * ffn, 6 * dim * ffn),
     )(*bs, wg, wu, wd, *after)
 
 
-def sum_kernel(*refs):
-    p_ref, t_ref, y_ref, z_ref = refs[-4:]
-    total = (p_ref[:].astype(F32) + t_ref[:].astype(F32)).astype(BF)
+def sum_kernel(*refs, n):
+    *parts, y_ref, z_ref = refs[-2 - n:]
+    total = sum(p[:].astype(F32) for p in parts).astype(BF)
     z_ref[:] = (y_ref[:].astype(F32) + total.astype(F32)).astype(BF)
 
 
-def sum_rows(z, mine, far, y, y_first, first, total, after=(), tile=64):
-    rows, dim = mine.shape
+def sum_rows(z, parts, y, y_first, first, total, after=(), tile=64):
+    rows, dim = parts[0].shape
     at = lambda r0: pl.BlockSpec((tile, dim), lambda i: (r0 // tile + i, 0))
     prev = () if z is None else (z,)
+    n = len(parts)
     return pl.pallas_call(
-        ordered(sum_kernel, len(prev) + 3, after), grid=(rows // tile,),
-        in_specs=[ANY] * len(prev) + [at(0), at(0), at(y_first)] + [ANY] * len(after),
+        ordered(functools.partial(sum_kernel, n=n), len(prev) + n + 1, after), grid=(rows // tile,),
+        in_specs=[ANY] * len(prev) + [at(0)] * n + [at(y_first)] + [ANY] * len(after),
         out_specs=at(first),
         out_shape=jax.ShapeDtypeStruct((total, dim), BF),
         input_output_aliases={0: 0} if prev else {},
         name="zsum", compiler_params=PARAMS,
-        cost_estimate=cost(rows * dim, 8 * rows * dim),
-    )(*prev, mine, far, y, *after)
+        cost_estimate=cost(rows * dim, rows * dim),
+    )(*prev, *parts, y, *after)
 
 
 def run_positions(xi, ci, y, cps, piece):
@@ -792,7 +830,7 @@
         rows = half // n_piece
         wo_c = send(over_core, tied(wo, kvs[-1]))
 
-        tiles = [(0, i) for i in range(2 * n_run)] + [(1, 0), (1, 1)]
+        tiles = [(0, i) for i in range(2 * n_run)] + [(1, i) for i in (0, 1)]
         st, *wo_x = flash(tab, [q_here, q_far[0]], tiles, kvs, base=bases[0], work=int(work[0]), cut=wo,
                          n_cut=n_piece)
         wo_x = [send(over_x, w) for w in wo_x]
@@ -826,7 +864,7 @@
 
         def project(i):
             ws = [wo, wo_c]
-            blocks = [[(0, 0, half)], [(0, half, half)], [(1, 0, half)], [(1, half, half)]]
+            blocks = [[(a, r, half)] for a in (0, 1) for r in (0, half)]
             for k in range(2):
                 for held in (wo_ya, wo_yb):
                     blocks.append([(len(ws) + p, 0, rows) for p in range(n_piece)])
@@ -856,14 +894,14 @@
 
         def finish(c):
             j, first, _ = chunks[c]
-            return sum_rows(z, *sums[c], outs[j][0], first, j * RUN + first, n_run * RUN,
+            return sum_rows(z, sums[c], outs[j][0], first, j * RUN + first, n_run * RUN,
                         after=() if prev is z else (prev,))
 
         relay_b(0)
         for c, (j, first, size) in enumerate(chunks):
             b = [outs[j][1], relay[j][0], outs[j][3], relay[j][1]]
-            prev, s_far = mlp(b, first, size, w_gate, w_up, w_down, c, after=(prev,))
-            sums.append((prev, send(over_x, s_far)))
+            prev, *s_far = mlp(b, first, size, w_gate, w_up, w_down, c, c == n_run, after=(prev,))
+            sums.append([prev] + [send(over_x, v) for v in s_far])
             if c < last:
                 relay_b(c + 1)
             if c == 0:

time: 1020 us -> 1010 us (level)
  waiting for transfers between devices: 174 us -> 151 us
  Pallas kernels: 773 us -> 784 us
    ppermute x49 -> x48, waiting for transfers between devices: 174 us -> 151 us  [send(): return lax.ppermute(v, *axis_pairs)]
    pallas_call x5, Pallas kernels: 374 us -> 385 us  [mlp(): pl.pallas_call(ordered(functools.partial(mlp_kernel, n_in=len(bs), first=...]
    ppermute x49 -> x48, starting transfers between devices: 39.8 us -> 39.4 us  [send(): return lax.ppermute(v, *axis_pairs)]
  transfers between devices with their start and end apart: 49 -> 48, of which waited for: 19 -> 18; matrix products, arithmetic and copies ran while one was open for 2% -> 2% of each run, Pallas kernels for 73% -> 75%
where the time goes in v14:
time: 1010 us; the launch traced here: 1000 us
  Pallas kernels  784 us (78%)
  waiting for transfers between devices  151 us (15%)
  starting transfers between devices  39.4 us (4%)
  local copies, waits for them, and re-layouts  18.8 us (2%)
    pallas_call x5, Pallas kernels, mlp(): pl.pallas_call(ordered(functools.partial(mlp_kernel, n_in=len(bs), first=...  385 us
    pallas_call x5, Pallas kernels, flash(): pl.pallas_call(ordered(functools.partial(flash_kernel, q_src=q_src, kv_sr...  211 us
    ppermute x48, waiting for transfers between devices, send(): return lax.ppermute(v, *axis_pairs)  151 us
    pallas_call x6, Pallas kernels, qkv(): pl.pallas_call(ordered(functools.partial(qkv_kernel, n_in=n_in, n_q=n_q,...  97.7 us
    pallas_call x2, Pallas kernels, out_proj(): pl.pallas_call(ordered(functools.partial(out_kernel, blocks=blocks, n_w=l...  58 us
    ppermute x48, starting transfers between devices, send(): return lax.ppermute(v, *axis_pairs)  39.4 us
  transfers between devices with their start and end apart: 48, of which 18 were waited for; matrix products, arithmetic and copies ran while one was open for 2% of the time, Pallas kernels for 75%

profile of v14, /device:TPU:0, one launch (start us, length us, event | category | flops | bytes accessed | tf_op | source)
XLA Modules:
  0.0 1000.5 jit_solution(4072350815373818086)
XLA Ops:
  1.3 3.4 norm.2.refs_2_.refs_0_
  4.8 3.3 collective-permute-start.5
  8.1 8.8 norm.3
  19.2 9.5 bitcast_dynamic-update-slice_fusion
  28.7 2.8 multiply_sine_fusion.1
  31.5 2.0 bitcast_dynamic-update-slice_fusion.2
  33.5 2.0 bitcast_dynamic-update-slice_fusion.1.refs_8_.refs_2_
  35.6 37.7 %qkv.6 = (bf16[8,1024,256]{2,1,0:T(8,128)(2,1)}, bf16[8,2,256,256]{3,2,1,0:T(8,128)(2,1)}) custom-call(bf16[256,4096]{1,0:T(8,128)(2,1)} %norm.2.refs_2_.refs_0_, bf16[256,4096]{1,0:T(8,128)(2,1)} %get-tuple-element.73.refs_1_, bf16[256,4096]{1,0:T(8,128)(2,1)} %get-tuple-element.74.refs_2_, bf16[256,4096]{1,0:T(8,128)(2,1)} %get-tuple-element.75.refs_3_, ...), custom_call_target="tpu_custom_call" | custom-call | flops 25769803776 | bytes 12582912 | tf_op jit(solution)/shard_map/qkv/pallas_call | solution.py:132
  74.1 3.4 multiply_sine_fusion
  77.8 14.0 %qkv.7 = (bf16[2,1024,256]{2,1,0:T(8,128)(2,1)}, bf16[2,2,256,256]{3,2,1,0:T(8,128)(2,1)}) custom-call(bf16[256,4096]{1,0:T(8,128)(2,1)} %collective-permute-done.5.refs_0_, bf16[256,4096]{1,0:T(8,128)(2,1)} %collective-permute-done.6.refs_1_, bf16[4096,1536]{1,0:T(8,128)(2,1)} %bitcast_dynamic-update-slice_fusion.1.refs_8_.refs_2_, ...), custom_call_target="tpu_custom_call" | custom-call | flops 6442450944 | bytes 12582912 | tf_op jit(solution)/shard_map/qkv/pallas_call | solution.py:132
  91.9 29.8 %collective-permute-done.4.refs_0_ = bf16[256,4096]{1,0:T(8,128)(2,1)} collective-permute-done((bf16[256,4096]{1,0:T(8,128)(2,1)}, bf16[256,4096]{1,0:T(8,128)(2,1)}, u32[]{:S(2)}, u32[]{:S(2)}) %collective-permute-start.4) | collective-permute-done | bytes 2097184 | tf_op jit(solution)/shard_map/ppermute | solution.py:797
  123.3 2.9 collective-permute-done.7.refs_1_
  126.2 13.6 %qkv.8 = (bf16[2,1024,256]{2,1,0:T(8,128)(2,1)}, bf16[2,2,256,256]{3,2,1,0:T(8,128)(2,1)}) custom-call(bf16[256,4096]{1,0:T(8,128)(2,1)} %collective-permute-done.4.refs_0_, bf16[256,4096]{1,0:T(8,128)(2,1)} %collective-permute-done.7.refs_1_, bf16[4096,1536]{1,0:T(8,128)(2,1)} %bitcast_dynamic-update-slice_fusion.1.refs_8_.refs_2_, ...), custom_call_target="tpu_custom_call" | custom-call | flops 6442450944 | bytes 12582912 | tf_op jit(solution)/shard_map/qkv/pallas_call | solution.py:132
  139.8 50.1 %flash_part.1 = (f32[10,2,4,144,256]{4,3,2,1,0:T(8,128)}, bf16[256,4096]{1,0:T(8,128)(2,1)}, bf16[256,4096]{1,0:T(8,128)(2,1)}) custom-call(s32[845]{0:T(1024)} %dynamic-slice_reduce_fusion.refs_0_, bf16[8,1024,256]{2,1,0:T(8,128)(2,1)} %get-tuple-element.80.refs_1_, bf16[2,1024,256]{2,1,0:T(8,128)(2,1)} %get-tuple-element.88.refs_2_, ...), custom_call_target="tpu_custom_call" | custom-call | flops 38654705664 | bytes 3145728 | tf_op jit(solution)/shard_map/flash_part/pallas_call | solution.py:391
  192.0 3.0 collective-permute-done.9.refs_1_
  195.0 13.8 %qkv.9 = (bf16[2,1024,256]{2,1,0:T(8,128)(2,1)}, bf16[2,2,256,256]{3,2,1,0:T(8,128)(2,1)}) custom-call(bf16[256,4096]{1,0:T(8,128)(2,1)} %collective-permute-done.8.refs_0_, bf16[256,4096]{1,0:T(8,128)(2,1)} %collective-permute-done.9.refs_1_, bf16[4096,1536]{1,0:T(8,128)(2,1)} %bitcast_dynamic-update-slice_fusion.1.refs_8_.refs_2_, ...), custom_call_target="tpu_custom_call" | custom-call | flops 6442450944 | bytes 12582912 | tf_op jit(solution)/shard_map/qkv/pallas_call | solution.py:132
  208.8 30.0 %collective-permute-done.10.refs_0_ = bf16[256,4096]{1,0:T(8,128)(2,1)} collective-permute-done((bf16[256,4096]{1,0:T(8,128)(2,1)}, bf16[256,4096]{1,0:T(8,128)(2,1)}, u32[]{:S(2)}, u32[]{:S(2)}) %collective-permute-start.10) | collective-permute-done | bytes 2097184 | tf_op jit(solution)/shard_map/ppermute | solution.py:797
  244.1 7.8 qkv.10.refs_5_.refs_7_
  253.5 10.8 %qkv.11.refs_14_.refs_2_ = bf16[2,1024,256]{2,1,0:T(8,128)(2,1)} custom-call(bf16[256,4096]{1,0:T(8,128)(2,1)} %collective-permute-done.10.refs_0_, bf16[256,4096]{1,0:T(8,128)(2,1)} %collective-permute-done.11.refs_1_, bf16[4096,1536]{1,0:T(8,128)(2,1)} %bitcast_dynamic-update-slice_fusion.1.refs_8_.refs_2_, f32[8,64,256]{2,1,0:T(8,128)} %get-tuple-element.144.refs_3_, ...), custom_call_target="tpu_custom_call" | custom-call | flops 6442450944 | bytes 12582912 | tf_op jit(solution)/shard_map/qkv/pallas_call | solution.py:132
  264.3 23.3 %collective-permute-done.12.refs_8_ = bf16[8,2,256,256]{3,2,1,0:T(8,128)(2,1)} collective-permute-done((bf16[8,2,256,256]{3,2,1,0:T(8,128)(2,1)}, bf16[8,2,256,256]{3,2,1,0:T(8,128)(2,1)}, u32[]{:S(2)}, u32[]{:S(2)}) %collective-permute-start.12) | collective-permute-done | bytes 2097184 | tf_op jit(solution)/shard_map/ppermute | solution.py:797
  287.6 11.2 %collective-permute-done.13.refs_9_ = bf16[2,2,256,256]{3,2,1,0:T(8,128)(2,1)} collective-permute-done((bf16[2,2,256,256]{3,2,1,0:T(8,128)(2,1)}, bf16[2,2,256,256]{3,2,1,0:T(8,128)(2,1)}, u32[]{:S(2)}, u32[]{:S(2)}) %collective-permute-start.13) | collective-permute-done | bytes 524320 | tf_op jit(solution)/shard_map/ppermute | solution.py:797
  300.4 9.7 collective-permute-done.14.refs_10_
  311.6 9.7 collective-permute-done.15.refs_11_
  321.3 10.8 %collective-permute-done.16.refs_12_ = bf16[2,2,256,256]{3,2,1,0:T(8,128)(2,1)} collective-permute-done((bf16[2,2,256,256]{3,2,1,0:T(8,128)(2,1)}, bf16[2,2,256,256]{3,2,1,0:T(8,128)(2,1)}, u32[]{:S(2)}, u32[]{:S(2)}) %collective-permute-start.16) | collective-permute-done | bytes 524320 | tf_op jit(solution)/shard_map/ppermute | solution.py:797
  332.1 29.1 %flash.4 = (bf16[2,256,1024]{2,1,0:T(8,128)(2,1)}, bf16[2,256,1024]{2,1,0:T(8,128)(2,1)}, bf16[2,256,1024]{2,1,0:T(8,128)(2,1)}, bf16[2,256,1024]{2,1,0:T(8,128)(2,1)}, f32[8,128]{1,0:T(8,128)}) custom-call(s32[845]{0:T(1024)} %dynamic-slice_reduce_fusion.refs_0_, bf16[8,1024,256]{2,1,0:T(8,128)(2,1)} %get-tuple-element.80.refs_1_, ...), custom_call_target="tpu_custom_call" | custom-call | flops 23622320128 | bytes 8388608 | tf_op jit(solution)/shard_map/flash/pallas_call | solution.py:391
  362.1 43.9 %flash.5 = (bf16[2,256,1024]{2,1,0:T(8,128)(2,1)}, bf16[2,256,1024]{2,1,0:T(8,128)(2,1)}, bf16[2,256,1024]{2,1,0:T(8,128)(2,1)}, bf16[2,256,1024]{2,1,0:T(8,128)(2,1)}, f32[8,128]{1,0:T(8,128)}) custom-call(s32[845]{0:T(1024)} %dynamic-slice_reduce_fusion.refs_0_, ...), custom_call_target="tpu_custom_call", output_to_operand_aliasing={{0}: (14, {}), {1}: (15, {}), {2}: (16, {}), {3}: (17, {})} | custom-call | flops 32212254720 | bytes 8388608 | tf_op jit(solution)/shard_map/flash/pallas_call | solution.py:391
  409.6 43.8 %flash.6 = (bf16[2,256,1024]{2,1,0:T(8,128)(2,1)}, bf16[2,256,1024]{2,1,0:T(8,128)(2,1)}, bf16[2,256,1024]{2,1,0:T(8,128)(2,1)}, bf16[2,256,1024]{2,1,0:T(8,128)(2,1)}, f32[8,128]{1,0:T(8,128)}) custom-call(s32[845]{0:T(1024)} %dynamic-slice_reduce_fusion.refs_0_, bf16[8,1024,256]{2,1,0:T(8,128)(2,1)} %get-tuple-element.80.refs_1_, ...), custom_call_target="tpu_custom_call" | custom-call | flops 32212254720 | bytes 8388608 | tf_op jit(solution)/shard_map/flash/pallas_call | solution.py:391
  453.5 2.6 collective-permute-done.24.refs_9_
  457.1 3.5 collective-permute-done.25.refs_10_
  460.6 3.0 collective-permute-done.26.refs_11_
  463.6 3.0 collective-permute-done.27.refs_12_
  466.5 3.0 collective-permute-done.28.refs_13_
  469.5 29.0 %outp.2 = (bf16[256,4096]{1,0:T(8,128)(2,1)}, bf16[256,4096]{1,0:T(8,128)(2,1)}, bf16[256,4096]{1,0:T(8,128)(2,1)}, bf16[256,4096]{1,0:T(8,128)(2,1)}) custom-call(bf16[2,256,1024]{2,1,0:T(8,128)(2,1)} %get-tuple-element.98.refs_0_, bf16[2,256,1024]{2,1,0:T(8,128)(2,1)} %collective-permute-done.17.refs_1_, ...), custom_call_target="tpu_custom_call" | custom-call | flops 17179869184 | bytes 33554432 | tf_op jit(solution)/shard_map/outp/pallas_call | solution.py:502
  498.8 7.2 collective-permute-start.29
  506.0 43.9 %flash.7 = (bf16[2,256,1024]{2,1,0:T(8,128)(2,1)}, bf16[2,256,1024]{2,1,0:T(8,128)(2,1)}, bf16[2,256,1024]{2,1,0:T(8,128)(2,1)}, bf16[2,256,1024]{2,1,0:T(8,128)(2,1)}, f32[8,128]{1,0:T(8,128)}) custom-call(s32[845]{0:T(1024)} %dynamic-slice_reduce_fusion.refs_0_, ...), custom_call_target="tpu_custom_call", output_to_operand_aliasing={{0}: (14, {}), {1}: (15, {}), {2}: (16, {}), {3}: (17, {})} | custom-call | flops 32212254720 | bytes 8388608 | tf_op jit(solution)/shard_map/flash/pallas_call | solution.py:391
  549.9 2.6 collective-permute-done.29.refs_1_
  555.0 2.0 collective-permute-done.31.refs_3_
  558.5 91.3 %mlp.5 = (bf16[256,4096]{1,0:T(8,128)(2,1)}, bf16[256,4096]{1,0:T(8,128)(2,1)}) custom-call(bf16[256,4096]{1,0:T(8,128)(2,1)} %get-tuple-element.112.refs_0_, bf16[256,4096]{1,0:T(8,128)(2,1)} %collective-permute-done.29.refs_1_, bf16[256,4096]{1,0:T(8,128)(2,1)} %collective-permute-done.30.refs_2_, bf16[256,4096]{1,0:T(8,128)(2,1)} %collective-permute-done.31.refs_3_, ...), custom_call_target="tpu_custom_call" | custom-call | flops 77309411328 | bytes 75497472 | tf_op jit(solution)/shard_map/mlp/pallas_call | solution.py:657
  650.0 29.0 %outp.3 = (bf16[256,4096]{1,0:T(8,128)(2,1)}, bf16[256,4096]{1,0:T(8,128)(2,1)}, bf16[256,4096]{1,0:T(8,128)(2,1)}, bf16[256,4096]{1,0:T(8,128)(2,1)}) custom-call(bf16[2,256,1024]{2,1,0:T(8,128)(2,1)} %get-tuple-element.124.refs_0_, bf16[2,256,1024]{2,1,0:T(8,128)(2,1)} %collective-permute-done.36.refs_1_, ...), custom_call_target="tpu_custom_call" | custom-call | flops 17179869184 | bytes 33554432 | tf_op jit(solution)/shard_map/outp/pallas_call | solution.py:502
  681.4 91.1 %mlp.6 = (bf16[256,4096]{1,0:T(8,128)(2,1)}, bf16[256,4096]{1,0:T(8,128)(2,1)}) custom-call(bf16[256,4096]{1,0:T(8,128)(2,1)} %get-tuple-element.122.refs_0_, bf16[256,4096]{1,0:T(8,128)(2,1)} %collective-permute-done.33.refs_1_, bf16[256,4096]{1,0:T(8,128)(2,1)} %collective-permute-done.34.refs_2_, bf16[256,4096]{1,0:T(8,128)(2,1)} %collective-permute-done.35.refs_3_, ...), custom_call_target="tpu_custom_call" | custom-call | flops 77309411328 | bytes 75497472 | tf_op jit(solution)/shard_map/mlp/pallas_call | solution.py:657
  775.2 4.9 zsum.5.refs_7_.refs_0_
  780.1 90.9 %mlp.7 = (bf16[256,4096]{1,0:T(8,128)(2,1)}, bf16[256,4096]{1,0:T(8,128)(2,1)}) custom-call(bf16[256,4096]{1,0:T(8,128)(2,1)} %get-tuple-element.132.refs_0_, bf16[256,4096]{1,0:T(8,128)(2,1)} %collective-permute-done.40.refs_1_, bf16[256,4096]{1,0:T(8,128)(2,1)} %collective-permute-done.41.refs_2_, bf16[256,4096]{1,0:T(8,128)(2,1)} %collective-permute-done.42.refs_3_, ...), custom_call_target="tpu_custom_call" | custom-call | flops 77309411328 | bytes 75497472 | tf_op jit(solution)/shard_map/mlp/pallas_call | solution.py:657
  871.9 4.9 zsum.6.refs_7_.refs_0_
  876.8 50.1 %mlp.8 = (bf16[128,4096]{1,0:T(8,128)(2,1)}, bf16[128,4096]{1,0:T(8,128)(2,1)}) custom-call(bf16[256,4096]{1,0:T(8,128)(2,1)} %get-tuple-element.136.refs_0_, bf16[256,4096]{1,0:T(8,128)(2,1)} %collective-permute-done.44.refs_1_, bf16[256,4096]{1,0:T(8,128)(2,1)} %collective-permute-done.45.refs_2_, bf16[256,4096]{1,0:T(8,128)(2,1)} %collective-permute-done.46.refs_3_, ...), custom_call_target="tpu_custom_call" | custom-call | flops 38654705664 | bytes 75497472 | tf_op jit(solution)/shard_map/mlp/pallas_call | solution.py:657
  928.7 4.9 zsum.7.refs_7_.refs_0_
  933.7 61.2 %mlp.9.refs_4_.refs_1_ = bf16[128,4096]{1,0:T(8,128)(2,1)} custom-call(bf16[256,4096]{1,0:T(8,128)(2,1)} %get-tuple-element.136.refs_0_, bf16[256,4096]{1,0:T(8,128)(2,1)} %collective-permute-done.44.refs_1_, bf16[256,4096]{1,0:T(8,128)(2,1)} %collective-permute-done.45.refs_2_, bf16[256,4096]{1,0:T(8,128)(2,1)} %collective-permute-done.46.refs_3_, ...), custom_call_target="tpu_custom_call" | custom-call | flops 38654705664 | bytes 75497472 | tf_op jit(solution)/shard_map/mlp/pallas_call | solution.py:657
  994.9 2.9 zsum.8.refs_0_
  997.8 2.4 zsum.9
  (93 shorter events, 36.2 us)
Async XLA Ops:
  4.8 68.5 %collective-permute-start.5 = (bf16[256,4096]{1,0:T(8,128)(2,1)}, bf16[256,4096]{1,0:T(8,128)(2,1)}, u32[]{:S(2)}, u32[]{:S(2)}) collective-permute-start(bf16[256,4096]{1,0:T(8,128)(2,1)} %norm.2.refs_2_.refs_0_), channel_id=1, source_target_pairs={{0,2},{1,3},{2,0},{3,1},{4,6},{5,7},{6,4},{7,5}} | collective-permute-start | bytes 6291464 | tf_op jit(solution)/shard_map/ppermute | solution.py:797
  8.1 27.5 %collective-permute-start = (bf16[256,4096]{1,0:T(8,128)(2,1)}, bf16[256,4096]{1,0:T(8,128)(2,1)}, u32[]{:S(2)}, u32[]{:S(2)}) collective-permute-start(bf16[256,4096]{1,0:T(8,128)(2,1)} %norm.2.refs_2_.refs_0_), channel_id=1, source_target_pairs={{0,1},{1,0},{2,3},{3,2},{4,5},{5,4},{6,7},{7,6}} | collective-permute-start | bytes 6291464 | tf_op jit(solution)/shard_map/ppermute | solution.py:797
  16.8 18.8 %collective-permute-start.1 = (bf16[256,4096]{1,0:T(8,128)(2,1)}, bf16[256,4096]{1,0:T(8,128)(2,1)}, u32[]{:S(2)}, u32[]{:S(2)}) collective-permute-start(bf16[256,4096]{1,0:T(8,128)(2,1)} %get-tuple-element.73.refs_1_), channel_id=1, source_target_pairs={{0,1},{1,0},{2,3},{3,2},{4,5},{5,4},{6,7},{7,6}} | collective-permute-start | bytes 6291464 | tf_op jit(solution)/shard_map/ppermute | solution.py:797
  17.3 18.3 %collective-permute-start.2 = (bf16[256,4096]{1,0:T(8,128)(2,1)}, bf16[256,4096]{1,0:T(8,128)(2,1)}, u32[]{:S(2)}, u32[]{:S(2)}) collective-permute-start(bf16[256,4096]{1,0:T(8,128)(2,1)} %get-tuple-element.74.refs_2_), channel_id=1, source_target_pairs={{0,1},{1,0},{2,3},{3,2},{4,5},{5,4},{6,7},{7,6}} | collective-permute-start | bytes 6291464 | tf_op jit(solution)/shard_map/ppermute | solution.py:797
  17.3 18.3 %collective-permute-start.3 = (bf16[256,4096]{1,0:T(8,128)(2,1)}, bf16[256,4096]{1,0:T(8,128)(2,1)}, u32[]{:S(2)}, u32[]{:S(2)}) collective-permute-start(bf16[256,4096]{1,0:T(8,128)(2,1)} %get-tuple-element.75.refs_3_), channel_id=1, source_target_pairs={{0,1},{1,0},{2,3},{3,2},{4,5},{5,4},{6,7},{7,6}} | collective-permute-start | bytes 6291464 | tf_op jit(solution)/shard_map/ppermute | solution.py:797
  73.3 4.5 collective-permute-start.6
  73.3 48.3 %collective-permute-start.4 = (bf16[256,4096]{1,0:T(8,128)(2,1)}, bf16[256,4096]{1,0:T(8,128)(2,1)}, u32[]{:S(2)}, u32[]{:S(2)}) collective-permute-start(bf16[256,4096]{1,0:T(8,128)(2,1)} %get-tuple-element.73.refs_1_), channel_id=1, source_target_pairs={{0,2},{1,3},{2,0},{3,1},{4,6},{5,7},{6,4},{7,5}} | collective-permute-start | bytes 6291464 | tf_op jit(solution)/shard_map/ppermute | solution.py:797
  121.7 4.5 collective-permute-start.7
  121.7 68.2 %collective-permute-start.8 = (bf16[256,4096]{1,0:T(8,128)(2,1)}, bf16[256,4096]{1,0:T(8,128)(2,1)}, u32[]{:S(2)}, u32[]{:S(2)}) collective-permute-start(bf16[256,4096]{1,0:T(8,128)(2,1)} %get-tuple-element.74.refs_2_), channel_id=1, source_target_pairs={{0,2},{1,3},{2,0},{3,1},{4,6},{5,7},{6,4},{7,5}} | collective-permute-start | bytes 6291464 | tf_op jit(solution)/shard_map/ppermute | solution.py:797
  189.9 5.1 collective-permute-start.9
  190.9 47.9 %collective-permute-start.10 = (bf16[256,4096]{1,0:T(8,128)(2,1)}, bf16[256,4096]{1,0:T(8,128)(2,1)}, u32[]{:S(2)}, u32[]{:S(2)}) collective-permute-start(bf16[256,4096]{1,0:T(8,128)(2,1)} %get-tuple-element.75.refs_3_), channel_id=1, source_target_pairs={{0,2},{1,3},{2,0},{3,1},{4,6},{5,7},{6,4},{7,5}} | collective-permute-start | bytes 6291464 | tf_op jit(solution)/shard_map/ppermute | solution.py:797
  238.8 5.4 collective-permute-start.11
  238.8 48.8 %collective-permute-start.12 = (bf16[8,2,256,256]{3,2,1,0:T(8,128)(2,1)}, bf16[8,2,256,256]{3,2,1,0:T(8,128)(2,1)}, u32[]{:S(2)}, u32[]{:S(2)}) collective-permute-start(bf16[8,2,256,256]{3,2,1,0:T(8,128)(2,1)} %get-tuple-element.81.refs_5_.refs_3_), channel_id=1, source_target_pairs={{0,4},{4,0},{1,5},{5,1},{2,6},{6,2},{3,7},{7,3}} | collective-permute-start | bytes 6291464 | tf_op jit(solution)/shard_map/ppermute | solution.py:797
  241.6 57.2 %collective-permute-start.13 = (bf16[2,2,256,256]{3,2,1,0:T(8,128)(2,1)}, bf16[2,2,256,256]{3,2,1,0:T(8,128)(2,1)}, u32[]{:S(2)}, u32[]{:S(2)}) collective-permute-start(bf16[2,2,256,256]{3,2,1,0:T(8,128)(2,1)} %get-tuple-element.84.refs_5_.refs_4_), channel_id=1, source_target_pairs={{0,4},{4,0},{1,5},{5,1},{2,6},{6,2},{3,7},{7,3}} | collective-permute-start | bytes 1572872 | tf_op jit(solution)/shard_map/ppermute | solution.py:797
  242.1 68.0 %collective-permute-start.14 = (bf16[2,2,256,256]{3,2,1,0:T(8,128)(2,1)}, bf16[2,2,256,256]{3,2,1,0:T(8,128)(2,1)}, u32[]{:S(2)}, u32[]{:S(2)}) collective-permute-start(bf16[2,2,256,256]{3,2,1,0:T(8,128)(2,1)} %get-tuple-element.87.refs_5_), channel_id=1, source_target_pairs={{0,4},{4,0},{1,5},{5,1},{2,6},{6,2},{3,7},{7,3}} | collective-permute-start | bytes 1572872 | tf_op jit(solution)/shard_map/ppermute | solution.py:797
  243.7 77.6 %collective-permute-start.15 = (bf16[2,2,256,256]{3,2,1,0:T(8,128)(2,1)}, bf16[2,2,256,256]{3,2,1,0:T(8,128)(2,1)}, u32[]{:S(2)}, u32[]{:S(2)}) collective-permute-start(bf16[2,2,256,256]{3,2,1,0:T(8,128)(2,1)} %get-tuple-element.91.refs_5_.refs_6_), channel_id=1, source_target_pairs={{0,4},{4,0},{1,5},{5,1},{2,6},{6,2},{3,7},{7,3}} | collective-permute-start | bytes 1572872 | tf_op jit(solution)/shard_map/ppermute | solution.py:797
  252.0 80.1 %collective-permute-start.16 = (bf16[2,2,256,256]{3,2,1,0:T(8,128)(2,1)}, bf16[2,2,256,256]{3,2,1,0:T(8,128)(2,1)}, u32[]{:S(2)}, u32[]{:S(2)}) collective-permute-start(bf16[2,2,256,256]{3,2,1,0:T(8,128)(2,1)} %qkv.10.refs_5_.refs_7_), channel_id=1, source_target_pairs={{0,4},{4,0},{1,5},{5,1},{2,6},{6,2},{3,7},{7,3}} | collective-permute-start | bytes 1572872 | tf_op jit(solution)/shard_map/ppermute | solution.py:797
  287.6 176.0 %collective-permute-start.20 = (bf16[1024,4096]{1,0:T(8,128)(2,1)}, bf16[1024,4096]{1,0:T(8,128)(2,1)}, u32[]{:S(2)}, u32[]{:S(2)}) collective-permute-start(bf16[1024,4096]{1,0:T(8,128)(2,1)} %bitcast.22), channel_id=1, source_target_pairs={{0,1},{1,0},{2,3},{3,2},{4,5},{5,4},{6,7},{7,6}} | collective-permute-start | bytes 25165832 | tf_op jit(solution)/shard_map/ppermute | solution.py:797
  298.8 62.4 %collective-permute-start.21 = (bf16[256,4096]{1,0:T(8,128)(2,1)}, bf16[256,4096]{1,0:T(8,128)(2,1)}, u32[]{:S(2)}, u32[]{:S(2)}) collective-permute-start(bf16[256,4096]{1,0:T(8,128)(2,1)} %get-tuple-element.103), channel_id=1, source_target_pairs={{0,2},{1,3},{2,0},{3,1},{4,6},{5,7},{6,4},{7,5}} | collective-permute-start | bytes 6291464 | tf_op jit(solution)/shard_map/ppermute | solution.py:797
  310.1 95.9 %collective-permute-start.22 = (bf16[256,4096]{1,0:T(8,128)(2,1)}, bf16[256,4096]{1,0:T(8,128)(2,1)}, u32[]{:S(2)}, u32[]{:S(2)}) collective-permute-start(bf16[256,4096]{1,0:T(8,128)(2,1)} %get-tuple-element.105), channel_id=1, source_target_pairs={{0,2},{1,3},{2,0},{3,1},{4,6},{5,7},{6,4},{7,5}} | collective-permute-start | bytes 6291464 | tf_op jit(solution)/shard_map/ppermute | solution.py:797
  361.2 47.5 %collective-permute-start.23 = (bf16[256,4096]{1,0:T(8,128)(2,1)}, bf16[256,4096]{1,0:T(8,128)(2,1)}, u32[]{:S(2)}, u32[]{:S(2)}) collective-permute-start(bf16[256,4096]{1,0:T(8,128)(2,1)} %collective-permute-done.21.refs_6_), channel_id=1, source_target_pairs={{0,4},{4,0},{1,5},{5,1},{2,6},{6,2},{3,7},{7,3}} | collective-permute-start | bytes 6291464 | tf_op jit(solution)/shard_map/ppermute | solution.py:797
  406.0 50.1 %collective-permute-start.17 = (bf16[2,256,1024]{2,1,0:T(8,128)(2,1)}, bf16[2,256,1024]{2,1,0:T(8,128)(2,1)}, u32[]{:S(2)}, u32[]{:S(2)}) collective-permute-start(bf16[2,256,1024]{2,1,0:T(8,128)(2,1)} %get-tuple-element.99), channel_id=1, source_target_pairs={{0,1},{1,0},{2,3},{3,2},{4,5},{5,4},{6,7},{7,6}} | collective-permute-start | bytes 3145736 | tf_op jit(solution)/shard_map/ppermute | solution.py:797
  406.0 50.5 %collective-permute-start.18 = (bf16[2,256,1024]{2,1,0:T(8,128)(2,1)}, bf16[2,256,1024]{2,1,0:T(8,128)(2,1)}, u32[]{:S(2)}, u32[]{:S(2)}) collective-permute-start(bf16[2,256,1024]{2,1,0:T(8,128)(2,1)} %get-tuple-element.100), channel_id=1, source_target_pairs={{0,2},{1,3},{2,0},{3,1},{4,6},{5,7},{6,4},{7,5}} | collective-permute-start | bytes 3145736 | tf_op jit(solution)/shard_map/ppermute | solution.py:797
  406.9 49.7 %collective-permute-start.19 = (bf16[2,256,1024]{2,1,0:T(8,128)(2,1)}, bf16[2,256,1024]{2,1,0:T(8,128)(2,1)}, u32[]{:S(2)}, u32[]{:S(2)}) collective-permute-start(bf16[2,256,1024]{2,1,0:T(8,128)(2,1)} %get-tuple-element.101), channel_id=1, source_target_pairs={{0,3},{1,2},{2,1},{3,0},{4,7},{5,6},{6,5},{7,4}} | collective-permute-start | bytes 3145736 | tf_op jit(solution)/shard_map/ppermute | solution.py:797
  408.7 47.3 %collective-permute-start.24 = (bf16[256,4096]{1,0:T(8,128)(2,1)}, bf16[256,4096]{1,0:T(8,128)(2,1)}, u32[]{:S(2)}, u32[]{:S(2)}) collective-permute-start(bf16[256,4096]{1,0:T(8,128)(2,1)} %collective-permute-done.22.refs_7_), channel_id=1, source_target_pairs={{0,4},{4,0},{1,5},{5,1},{2,6},{6,2},{3,7},{7,3}} | collective-permute-start | bytes 6291464 | tf_op jit(solution)/shard_map/ppermute | solution.py:797
  456.0 4.5 collective-permute-start.25
  456.1 7.5 collective-permute-start.26
  456.6 10.0 collective-permute-start.27
  456.6 13.0 %collective-permute-start.28 = (bf16[256,4096]{1,0:T(8,128)(2,1)}, bf16[256,4096]{1,0:T(8,128)(2,1)}, u32[]{:S(2)}, u32[]{:S(2)}) collective-permute-start(bf16[256,4096]{1,0:T(8,128)(2,1)} %collective-permute-done.24.refs_9_), channel_id=1, source_target_pairs={{0,1},{1,0},{2,3},{3,2},{4,5},{5,4},{6,7},{7,6}} | collective-permute-start | bytes 6291464 | tf_op jit(solution)/shard_map/ppermute | solution.py:797
  498.6 56.1 %collective-permute-start.30 = (bf16[256,4096]{1,0:T(8,128)(2,1)}, bf16[256,4096]{1,0:T(8,128)(2,1)}, u32[]{:S(2)}, u32[]{:S(2)}) collective-permute-start(bf16[256,4096]{1,0:T(8,128)(2,1)} %get-tuple-element.112.refs_0_), channel_id=1, source_target_pairs={{0,1},{1,0},{2,3},{3,2},{4,5},{5,4},{6,7},{7,6}} | collective-permute-start | bytes 6291464 | tf_op jit(solution)/shard_map/ppermute | solution.py:797
  498.8 53.7 %collective-permute-start.29 = (bf16[256,4096]{1,0:T(8,128)(2,1)}, bf16[256,4096]{1,0:T(8,128)(2,1)}, u32[]{:S(2)}, u32[]{:S(2)}) collective-permute-start(bf16[256,4096]{1,0:T(8,128)(2,1)} %get-tuple-element.112.refs_0_), channel_id=1, source_target_pairs={{0,2},{1,3},{2,0},{3,1},{4,6},{5,7},{6,4},{7,5}} | collective-permute-start | bytes 6291464 | tf_op jit(solution)/shard_map/ppermute | solution.py:797
  552.5 4.5 collective-permute-start.31
  552.5 128.9 %collective-permute-start.34 = (bf16[256,4096]{1,0:T(8,128)(2,1)}, bf16[256,4096]{1,0:T(8,128)(2,1)}, u32[]{:S(2)}, u32[]{:S(2)}) collective-permute-start(bf16[256,4096]{1,0:T(8,128)(2,1)} %get-tuple-element.122.refs_0_), channel_id=1, source_target_pairs={{0,1},{1,0},{2,3},{3,2},{4,5},{5,4},{6,7},{7,6}} | collective-permute-start | bytes 6291464 | tf_op jit(solution)/shard_map/ppermute | solution.py:797
  553.0 96.8 %collective-permute-start.33 = (bf16[256,4096]{1,0:T(8,128)(2,1)}, bf16[256,4096]{1,0:T(8,128)(2,1)}, u32[]{:S(2)}, u32[]{:S(2)}) collective-permute-start(bf16[256,4096]{1,0:T(8,128)(2,1)} %get-tuple-element.122.refs_0_), channel_id=1, source_target_pairs={{0,2},{1,3},{2,0},{3,1},{4,6},{5,7},{6,4},{7,5}} | collective-permute-start | bytes 6291464 | tf_op jit(solution)/shard_map/ppermute | solution.py:797
  554.7 95.2 %collective-permute-start.36 = (bf16[2,256,1024]{2,1,0:T(8,128)(2,1)}, bf16[2,256,1024]{2,1,0:T(8,128)(2,1)}, u32[]{:S(2)}, u32[]{:S(2)}) collective-permute-start(bf16[2,256,1024]{2,1,0:T(8,128)(2,1)} %get-tuple-element.125), channel_id=1, source_target_pairs={{0,1},{1,0},{2,3},{3,2},{4,5},{5,4},{6,7},{7,6}} | collective-permute-start | bytes 3145736 | tf_op jit(solution)/shard_map/ppermute | solution.py:797
  554.7 95.2 %collective-permute-start.37 = (bf16[2,256,1024]{2,1,0:T(8,128)(2,1)}, bf16[2,256,1024]{2,1,0:T(8,128)(2,1)}, u32[]{:S(2)}, u32[]{:S(2)}) collective-permute-start(bf16[2,256,1024]{2,1,0:T(8,128)(2,1)} %get-tuple-element.126), channel_id=1, source_target_pairs={{0,2},{1,3},{2,0},{3,1},{4,6},{5,7},{6,4},{7,5}} | collective-permute-start | bytes 3145736 | tf_op jit(solution)/shard_map/ppermute | solution.py:797
  557.0 93.0 %collective-permute-start.38 = (bf16[2,256,1024]{2,1,0:T(8,128)(2,1)}, bf16[2,256,1024]{2,1,0:T(8,128)(2,1)}, u32[]{:S(2)}, u32[]{:S(2)}) collective-permute-start(bf16[2,256,1024]{2,1,0:T(8,128)(2,1)} %get-tuple-element.127), channel_id=1, source_target_pairs={{0,3},{1,2},{2,1},{3,0},{4,7},{5,6},{6,5},{7,4}} | collective-permute-start | bytes 3145736 | tf_op jit(solution)/shard_map/ppermute | solution.py:797
  649.8 31.6 %collective-permute-start.35 = (bf16[256,4096]{1,0:T(8,128)(2,1)}, bf16[256,4096]{1,0:T(8,128)(2,1)}, u32[]{:S(2)}, u32[]{:S(2)}) collective-permute-start(bf16[256,4096]{1,0:T(8,128)(2,1)} %collective-permute-done.33.refs_1_), channel_id=1, source_target_pairs={{0,1},{1,0},{2,3},{3,2},{4,5},{5,4},{6,7},{7,6}} | collective-permute-start | bytes 6291464 | tf_op jit(solution)/shard_map/ppermute | solution.py:797
  679.0 101.1 %collective-permute-start.41 = (bf16[256,4096]{1,0:T(8,128)(2,1)}, bf16[256,4096]{1,0:T(8,128)(2,1)}, u32[]{:S(2)}, u32[]{:S(2)}) collective-permute-start(bf16[256,4096]{1,0:T(8,128)(2,1)} %get-tuple-element.132.refs_0_), channel_id=1, source_target_pairs={{0,1},{1,0},{2,3},{3,2},{4,5},{5,4},{6,7},{7,6}} | collective-permute-start | bytes 6291464 | tf_op jit(solution)/shard_map/ppermute | solution.py:797
  679.4 93.2 %collective-permute-start.40 = (bf16[256,4096]{1,0:T(8,128)(2,1)}, bf16[256,4096]{1,0:T(8,128)(2,1)}, u32[]{:S(2)}, u32[]{:S(2)}) collective-permute-start(bf16[256,4096]{1,0:T(8,128)(2,1)} %get-tuple-element.132.refs_0_), channel_id=1, source_target_pairs={{0,2},{1,3},{2,0},{3,1},{4,6},{5,7},{6,4},{7,5}} | collective-permute-start | bytes 6291464 | tf_op jit(solution)/shard_map/ppermute | solution.py:797
  679.6 93.8 %collective-permute-start.32 = (bf16[256,4096]{1,0:T(8,128)(2,1)}, bf16[256,4096]{1,0:T(8,128)(2,1)}, u32[]{:S(2)}, u32[]{:S(2)}) collective-permute-start(bf16[256,4096]{1,0:T(8,128)(2,1)} %get-tuple-element.121), channel_id=1, source_target_pairs={{0,2},{1,3},{2,0},{3,1},{4,6},{5,7},{6,4},{7,5}} | collective-permute-start | bytes 6291464 | tf_op jit(solution)/shard_map/ppermute | solution.py:797
  772.5 7.6 collective-permute-start.42
  773.1 103.8 %collective-permute-start.45 = (bf16[256,4096]{1,0:T(8,128)(2,1)}, bf16[256,4096]{1,0:T(8,128)(2,1)}, u32[]{:S(2)}, u32[]{:S(2)}) collective-permute-start(bf16[256,4096]{1,0:T(8,128)(2,1)} %get-tuple-element.136.refs_0_), channel_id=1, source_target_pairs={{0,1},{1,0},{2,3},{3,2},{4,5},{5,4},{6,7},{7,6}} | collective-permute-start | bytes 6291464 | tf_op jit(solution)/shard_map/ppermute | solution.py:797
  773.1 97.9 %collective-permute-start.44 = (bf16[256,4096]{1,0:T(8,128)(2,1)}, bf16[256,4096]{1,0:T(8,128)(2,1)}, u32[]{:S(2)}, u32[]{:S(2)}) collective-permute-start(bf16[256,4096]{1,0:T(8,128)(2,1)} %get-tuple-element.136.refs_0_), channel_id=1, source_target_pairs={{0,2},{1,3},{2,0},{3,1},{4,6},{5,7},{6,4},{7,5}} | collective-permute-start | bytes 6291464 | tf_op jit(solution)/shard_map/ppermute | solution.py:797
  773.4 98.5 %collective-permute-start.39 = (bf16[256,4096]{1,0:T(8,128)(2,1)}, bf16[256,4096]{1,0:T(8,128)(2,1)}, u32[]{:S(2)}, u32[]{:S(2)}) collective-permute-start(bf16[256,4096]{1,0:T(8,128)(2,1)} %get-tuple-element.130), channel_id=1, source_target_pairs={{0,2},{1,3},{2,0},{3,1},{4,6},{5,7},{6,4},{7,5}} | collective-permute-start | bytes 6291464 | tf_op jit(solution)/shard_map/ppermute | solution.py:797
  871.0 5.8 collective-permute-start.46
  871.6 57.1 %collective-permute-start.43 = (bf16[256,4096]{1,0:T(8,128)(2,1)}, bf16[256,4096]{1,0:T(8,128)(2,1)}, u32[]{:S(2)}, u32[]{:S(2)}) collective-permute-start(bf16[256,4096]{1,0:T(8,128)(2,1)} %get-tuple-element.135), channel_id=1, source_target_pairs={{0,2},{1,3},{2,0},{3,1},{4,6},{5,7},{6,4},{7,5}} | collective-permute-start | bytes 6291464 | tf_op jit(solution)/shard_map/ppermute | solution.py:797
  927.0 67.9 %collective-permute-start.47 = (bf16[128,4096]{1,0:T(8,128)(2,1)}, bf16[128,4096]{1,0:T(8,128)(2,1)}, u32[]{:S(2)}, u32[]{:S(2)}) collective-permute-start(bf16[128,4096]{1,0:T(8,128)(2,1)} %get-tuple-element.139), channel_id=1, source_target_pairs={{0,2},{1,3},{2,0},{3,1},{4,6},{5,7},{6,4},{7,5}} | collective-permute-start | bytes 3145736 | tf_op jit(solution)/shard_map/ppermute | solution.py:797
  (3 other events, 25.2 us)

commit v15 on v14

--- a/solution.py
+++ b/solution.py
@@ -518,7 +518,7 @@
     b_refs = refs[:n_in]
     wg_ref, wu_ref, wd_ref, *outs = refs[n_in:n_in + (4 if cross else 5)]
     (b_scr, u_scr, w_scr, d_scr, keep_scr, out_scr, in_scr, b_sem, w_sem, d_sem, out_sem, in_sem,
-     *more) = refs[n_in + (4 if cross else 5):]
+     rows_sem, *more) = refs[n_in + (4 if cross else 5):]
     i = pl.program_id(0)
     me = lax.axis_index('tp')
     mate = {'tp': me + 1 - 2 * lax.rem(me, 2)}
@@ -555,20 +555,24 @@
         return pltpu.make_async_remote_copy(src_ref=far_scr.at[n], dst_ref=back_scr.at[n], send_sem=far_sem.at[n],
                                             recv_sem=back_sem.at[n], device_id=peers[-1], device_id_type=pl.DeviceIdType.MESH)
 
+    def rows_to_mate(n):
+        return pltpu.make_async_remote_copy(
+            src_ref=b_refs[n].at[pl.ds(first, rb), :], dst_ref=b_scr.at[pl.ds((n_in + n) * rb, rb), :],
+            send_sem=rows_sem.at[n], recv_sem=b_sem.at[n_in + n], device_id=mate, device_id_type=pl.DeviceIdType.MESH)
+
     @pl.when(i == 0)
     def _():
         copies = [pltpu.make_async_copy(r.at[pl.ds(first, rb), :], b_scr.at[pl.ds(k * rb, rb), :], b_sem.at[k])
                   for k, r in enumerate(b_refs)]
+        for peer in peers:
+            pl.semaphore_signal(barrier, inc=1, device_id=peer, device_id_type=pl.DeviceIdType.MESH)
         copies[0].start()
         fetch(i)
         for cp in copies[1:]:
             cp.start()
-        for peer in peers:
-            pl.semaphore_signal(barrier, inc=1, device_id=peer, device_id_type=pl.DeviceIdType.MESH)
-
-    @pl.when(i == 1)
-    def _():
         pl.semaphore_wait(barrier, len(peers))
+        for n in range(n_in):
+            rows_to_mate(n).start()
 
     fetch(i + 1)
 
@@ -585,7 +589,7 @@
             gated(rows, pl.ds(0, tn), 0)
             return carry
 
-        lax.fori_loop(0, n_in, one, 0)
+        lax.fori_loop(0, 2 * n_in, one, 0)
 
     @pl.when((i > 0) & (i < nk))
     def _():
@@ -640,11 +644,13 @@
             return carry
 
         lax.fori_loop(0, nd, sent, 0)
+        for k in range(n_in):
+            rows_to_mate(k).wait_send()
 
 
 def mlp(bs, first, rb, wg, wu, wd, call, cross=False, after=()):
     dim = bs[0].shape[1]
-    rows = rb * len(bs)
+    rows = 2 * rb * len(bs)
     ffn = wg.shape[1]
     td = 512
     tn = td if rows <= td else td // 2
@@ -663,7 +669,7 @@
         out_shape=[jax.ShapeDtypeStruct((rb, dim), BF)] * n_out,
         scratch_shapes=[pltpu.VMEM((rows, dim), BF), pltpu.VMEM((rows, ffn), BF), pltpu.VMEM((2, 2, dim, tn), BF),
                         pltpu.VMEM((2, ffn, td), BF), pltpu.VMEM((2, half, td), BF), tiles, tiles]
-        + [sem((n,)) for n in (len(bs), 2, 2, nd, nd)]
+        + [sem((n,)) for n in (2 * len(bs), 2, 2, nd, nd, len(bs))]
         + ([pltpu.VMEM((nd, rb, td), BF)] * 3 + [sem((nd,))] * 2 if cross else []),
         name="mlp",
         compiler_params=pltpu.CompilerParams(vmem_limit_bytes=VMEM, collective_id=call, has_side_effects=True),
@@ -871,7 +877,7 @@
                     ws += [held[p][k] for p in range(n_piece)]
             got = out_proj(os[i], ws, blocks, x_rows, gm, i, after=(prev,))
             for y, b in zip(got[::2], got[1::2]):
-                outs.append((y, b, send(over_x, b), send(over_core, b)))
+                outs.append((y, b, send(over_x, b)))
             return got[0]
 
         last = n_run - 1
@@ -884,11 +890,7 @@
         prev = project(0)
         prev = attend(last)
 
-        z, sums, relay = None, [], {}
-
-        def relay_b(j):
-            here = tied(outs[j][2], prev)
-            relay[j] = (here, send(over_core, here))
+        z, sums = None, []
 
         chunks = [(j, 0, RUN) for j in range(last)] + [(last, 0, RUN // 2), (last, RUN // 2, RUN // 2)]
 
@@ -897,13 +899,9 @@
             return sum_rows(z, sums[c], outs[j][0], first, j * RUN + first, n_run * RUN,
                         after=() if prev is z else (prev,))
 
-        relay_b(0)
         for c, (j, first, size) in enumerate(chunks):
-            b = [outs[j][1], relay[j][0], outs[j][3], relay[j][1]]
-            prev, *s_far = mlp(b, first, size, w_gate, w_up, w_down, c, c == n_run, after=(prev,))
+            prev, *s_far = mlp(outs[j][1:], first, size, w_gate, w_up, w_down, c, c == n_run, after=(prev,))
             sums.append([prev] + [send(over_x, v) for v in s_far])
-            if c < last:
-                relay_b(c + 1)
             if c == 0:
                 prev = project(1)
             elif c < n_run:

time: 1010 us -> 1040 us (1.030)
  waiting for transfers between devices: 151 us -> 191 us
    ppermute x48 -> x40, waiting for transfers between devices: 151 us -> 191 us  [send(): return lax.ppermute(v, *axis_pairs)]
    ppermute x48 -> x40, starting transfers between devices: 39.4 us -> 36.3 us  [send(): return lax.ppermute(v, *axis_pairs)]
  transfers between devices with their start and end apart: 48 -> 40, of which waited for: 18 -> 18; matrix products, arithmetic and copies ran while one was open for 2% -> 2% of each run, Pallas kernels for 75% -> 72%
where the time goes in v15:
time: 1040 us; the launch traced here: 1030 us
  Pallas kernels  781 us (75%)
  waiting for transfers between devices  191 us (18%)
  starting transfers between devices  36.3 us (3%)
  local copies, waits for them, and re-layouts  18.7 us (2%)
    pallas_call x5, Pallas kernels, mlp(): pl.pallas_call(ordered(functools.partial(mlp_kernel, n_in=len(bs), first=...  383 us
    pallas_call x5, Pallas kernels, flash(): pl.pallas_call(ordered(functools.partial(flash_kernel, q_src=q_src, kv_sr...  211 us
    ppermute x40, waiting for transfers between devices, send(): return lax.ppermute(v, *axis_pairs)  191 us
    pallas_call x6, Pallas kernels, qkv(): pl.pallas_call(ordered(functools.partial(qkv_kernel, n_in=n_in, n_q=n_q,...  97.7 us
    pallas_call x2, Pallas kernels, out_proj(): pl.pallas_call(ordered(functools.partial(out_kernel, blocks=blocks, n_w=l...  58 us
    ppermute x40, starting transfers between devices, send(): return lax.ppermute(v, *axis_pairs)  36.3 us
  transfers between devices with their start and end apart: 40, of which 18 were waited for; matrix products, arithmetic and copies ran while one was open for 2% of the time, Pallas kernels for 72%

profile of v15, /device:TPU:0, one launch (start us, length us, event | category | flops | bytes accessed | tf_op | source)
XLA Modules:
  0.0 1034.7 jit_solution(15022715933454756666)
XLA Ops:
  1.3 3.4 norm.2.refs_2_.refs_0_
  4.7 3.3 collective-permute-start.5
  8.0 8.6 norm.3
  19.1 9.5 bitcast_dynamic-update-slice_fusion
  28.5 2.8 multiply_sine_fusion.1
  31.3 2.0 bitcast_dynamic-update-slice_fusion.2
  35.3 37.6 %qkv.6 = (bf16[8,1024,256]{2,1,0:T(8,128)(2,1)}, bf16[8,2,256,256]{3,2,1,0:T(8,128)(2,1)}) custom-call(bf16[256,4096]{1,0:T(8,128)(2,1)} %norm.2.refs_2_.refs_0_, bf16[256,4096]{1,0:T(8,128)(2,1)} %get-tuple-element.69.refs_1_, bf16[256,4096]{1,0:T(8,128)(2,1)} %get-tuple-element.70.refs_2_, bf16[256,4096]{1,0:T(8,128)(2,1)} %get-tuple-element.71.refs_3_, ...), custom_call_target="tpu_custom_call" | custom-call | flops 25769803776 | bytes 12582912 | tf_op jit(solution)/shard_map/qkv/pallas_call | solution.py:132
  73.8 3.4 multiply_sine_fusion
  77.5 14.1 %qkv.7 = (bf16[2,1024,256]{2,1,0:T(8,128)(2,1)}, bf16[2,2,256,256]{3,2,1,0:T(8,128)(2,1)}) custom-call(bf16[256,4096]{1,0:T(8,128)(2,1)} %collective-permute-done.5.refs_0_, bf16[256,4096]{1,0:T(8,128)(2,1)} %collective-permute-done.6.refs_1_, bf16[4096,1536]{1,0:T(8,128)(2,1)} %bitcast_dynamic-update-slice_fusion.1.refs_8_.refs_2_, ...), custom_call_target="tpu_custom_call" | custom-call | flops 6442450944 | bytes 12582912 | tf_op jit(solution)/shard_map/qkv/pallas_call | solution.py:132
  91.6 29.8 %collective-permute-done.4.refs_0_ = bf16[256,4096]{1,0:T(8,128)(2,1)} collective-permute-done((bf16[256,4096]{1,0:T(8,128)(2,1)}, bf16[256,4096]{1,0:T(8,128)(2,1)}, u32[]{:S(2)}, u32[]{:S(2)}) %collective-permute-start.4) | collective-permute-done | bytes 2097184 | tf_op jit(solution)/shard_map/ppermute | solution.py:803
  123.0 2.9 collective-permute-done.7.refs_1_
  125.9 13.6 %qkv.8 = (bf16[2,1024,256]{2,1,0:T(8,128)(2,1)}, bf16[2,2,256,256]{3,2,1,0:T(8,128)(2,1)}) custom-call(bf16[256,4096]{1,0:T(8,128)(2,1)} %collective-permute-done.4.refs_0_, bf16[256,4096]{1,0:T(8,128)(2,1)} %collective-permute-done.7.refs_1_, bf16[4096,1536]{1,0:T(8,128)(2,1)} %bitcast_dynamic-update-slice_fusion.1.refs_8_.refs_2_, ...), custom_call_target="tpu_custom_call" | custom-call | flops 6442450944 | bytes 12582912 | tf_op jit(solution)/shard_map/qkv/pallas_call | solution.py:132
  139.5 50.0 %flash_part.1 = (f32[10,2,4,144,256]{4,3,2,1,0:T(8,128)}, bf16[256,4096]{1,0:T(8,128)(2,1)}, bf16[256,4096]{1,0:T(8,128)(2,1)}) custom-call(s32[845]{0:T(1024)} %dynamic-slice_reduce_fusion.refs_0_, bf16[8,1024,256]{2,1,0:T(8,128)(2,1)} %get-tuple-element.76.refs_1_, bf16[2,1024,256]{2,1,0:T(8,128)(2,1)} %get-tuple-element.84.refs_2_, ...), custom_call_target="tpu_custom_call" | custom-call | flops 38654705664 | bytes 3145728 | tf_op jit(solution)/shard_map/flash_part/pallas_call | solution.py:391
  191.6 3.0 collective-permute-done.9.refs_1_
  194.7 13.8 %qkv.9 = (bf16[2,1024,256]{2,1,0:T(8,128)(2,1)}, bf16[2,2,256,256]{3,2,1,0:T(8,128)(2,1)}) custom-call(bf16[256,4096]{1,0:T(8,128)(2,1)} %collective-permute-done.8.refs_0_, bf16[256,4096]{1,0:T(8,128)(2,1)} %collective-permute-done.9.refs_1_, bf16[4096,1536]{1,0:T(8,128)(2,1)} %bitcast_dynamic-update-slice_fusion.1.refs_8_.refs_2_, ...), custom_call_target="tpu_custom_call" | custom-call | flops 6442450944 | bytes 12582912 | tf_op jit(solution)/shard_map/qkv/pallas_call | solution.py:132
  208.5 30.0 %collective-permute-done.10.refs_0_ = bf16[256,4096]{1,0:T(8,128)(2,1)} collective-permute-done((bf16[256,4096]{1,0:T(8,128)(2,1)}, bf16[256,4096]{1,0:T(8,128)(2,1)}, u32[]{:S(2)}, u32[]{:S(2)}) %collective-permute-start.10) | collective-permute-done | bytes 2097184 | tf_op jit(solution)/shard_map/ppermute | solution.py:803
  243.8 7.8 qkv.10.refs_5_.refs_7_
  253.2 10.8 %qkv.11.refs_14_.refs_2_ = bf16[2,1024,256]{2,1,0:T(8,128)(2,1)} custom-call(bf16[256,4096]{1,0:T(8,128)(2,1)} %collective-permute-done.10.refs_0_, bf16[256,4096]{1,0:T(8,128)(2,1)} %collective-permute-done.11.refs_1_, bf16[4096,1536]{1,0:T(8,128)(2,1)} %bitcast_dynamic-update-slice_fusion.1.refs_8_.refs_2_, f32[8,64,256]{2,1,0:T(8,128)} %get-tuple-element.136.refs_3_, ...), custom_call_target="tpu_custom_call" | custom-call | flops 6442450944 | bytes 12582912 | tf_op jit(solution)/shard_map/qkv/pallas_call | solution.py:132
  264.0 23.2 %collective-permute-done.12.refs_8_ = bf16[8,2,256,256]{3,2,1,0:T(8,128)(2,1)} collective-permute-done((bf16[8,2,256,256]{3,2,1,0:T(8,128)(2,1)}, bf16[8,2,256,256]{3,2,1,0:T(8,128)(2,1)}, u32[]{:S(2)}, u32[]{:S(2)}) %collective-permute-start.12) | collective-permute-done | bytes 2097184 | tf_op jit(solution)/shard_map/ppermute | solution.py:803
  287.3 11.2 %collective-permute-done.13.refs_9_ = bf16[2,2,256,256]{3,2,1,0:T(8,128)(2,1)} collective-permute-done((bf16[2,2,256,256]{3,2,1,0:T(8,128)(2,1)}, bf16[2,2,256,256]{3,2,1,0:T(8,128)(2,1)}, u32[]{:S(2)}, u32[]{:S(2)}) %collective-permute-start.13) | collective-permute-done | bytes 524320 | tf_op jit(solution)/shard_map/ppermute | solution.py:803
  300.0 9.7 collective-permute-done.14.refs_10_
  311.3 9.7 collective-permute-done.15.refs_11_
  321.0 10.8 %collective-permute-done.16.refs_12_ = bf16[2,2,256,256]{3,2,1,0:T(8,128)(2,1)} collective-permute-done((bf16[2,2,256,256]{3,2,1,0:T(8,128)(2,1)}, bf16[2,2,256,256]{3,2,1,0:T(8,128)(2,1)}, u32[]{:S(2)}, u32[]{:S(2)}) %collective-permute-start.16) | collective-permute-done | bytes 524320 | tf_op jit(solution)/shard_map/ppermute | solution.py:803
  331.7 29.1 %flash.4 = (bf16[2,256,1024]{2,1,0:T(8,128)(2,1)}, bf16[2,256,1024]{2,1,0:T(8,128)(2,1)}, bf16[2,256,1024]{2,1,0:T(8,128)(2,1)}, bf16[2,256,1024]{2,1,0:T(8,128)(2,1)}, f32[8,128]{1,0:T(8,128)}) custom-call(s32[845]{0:T(1024)} %dynamic-slice_reduce_fusion.refs_0_, bf16[8,1024,256]{2,1,0:T(8,128)(2,1)} %get-tuple-element.76.refs_1_, ...), custom_call_target="tpu_custom_call" | custom-call | flops 23622320128 | bytes 8388608 | tf_op jit(solution)/shard_map/flash/pallas_call | solution.py:391
  361.8 43.8 %flash.5 = (bf16[2,256,1024]{2,1,0:T(8,128)(2,1)}, bf16[2,256,1024]{2,1,0:T(8,128)(2,1)}, bf16[2,256,1024]{2,1,0:T(8,128)(2,1)}, bf16[2,256,1024]{2,1,0:T(8,128)(2,1)}, f32[8,128]{1,0:T(8,128)}) custom-call(s32[845]{0:T(1024)} %dynamic-slice_reduce_fusion.refs_0_, ...), custom_call_target="tpu_custom_call", output_to_operand_aliasing={{0}: (14, {}), {1}: (15, {}), {2}: (16, {}), {3}: (17, {})} | custom-call | flops 32212254720 | bytes 8388608 | tf_op jit(solution)/shard_map/flash/pallas_call | solution.py:391
  409.3 43.9 %flash.6 = (bf16[2,256,1024]{2,1,0:T(8,128)(2,1)}, bf16[2,256,1024]{2,1,0:T(8,128)(2,1)}, bf16[2,256,1024]{2,1,0:T(8,128)(2,1)}, bf16[2,256,1024]{2,1,0:T(8,128)(2,1)}, f32[8,128]{1,0:T(8,128)}) custom-call(s32[845]{0:T(1024)} %dynamic-slice_reduce_fusion.refs_0_, bf16[8,1024,256]{2,1,0:T(8,128)(2,1)} %get-tuple-element.76.refs_1_, ...), custom_call_target="tpu_custom_call" | custom-call | flops 32212254720 | bytes 8388608 | tf_op jit(solution)/shard_map/flash/pallas_call | solution.py:391
  453.2 2.5 collective-permute-done.24.refs_9_
  456.8 3.5 collective-permute-done.25.refs_10_
  460.2 3.0 collective-permute-done.26.refs_11_
  463.2 3.0 collective-permute-done.27.refs_12_
  466.2 3.0 collective-permute-done.28.refs_13_
  469.2 29.0 %outp.2 = (bf16[256,4096]{1,0:T(8,128)(2,1)}, bf16[256,4096]{1,0:T(8,128)(2,1)}, bf16[256,4096]{1,0:T(8,128)(2,1)}, bf16[256,4096]{1,0:T(8,128)(2,1)}) custom-call(bf16[2,256,1024]{2,1,0:T(8,128)(2,1)} %get-tuple-element.94.refs_0_, bf16[2,256,1024]{2,1,0:T(8,128)(2,1)} %collective-permute-done.17.refs_1_, ...), custom_call_target="tpu_custom_call" | custom-call | flops 17179869184 | bytes 33554432 | tf_op jit(solution)/shard_map/outp/pallas_call | solution.py:502
  498.2 7.3 collective-permute-start.29
  505.5 43.8 %flash.7 = (bf16[2,256,1024]{2,1,0:T(8,128)(2,1)}, bf16[2,256,1024]{2,1,0:T(8,128)(2,1)}, bf16[2,256,1024]{2,1,0:T(8,128)(2,1)}, bf16[2,256,1024]{2,1,0:T(8,128)(2,1)}, f32[8,128]{1,0:T(8,128)}) custom-call(s32[845]{0:T(1024)} %dynamic-slice_reduce_fusion.refs_0_, ...), custom_call_target="tpu_custom_call", output_to_operand_aliasing={{0}: (14, {}), {1}: (15, {}), {2}: (16, {}), {3}: (17, {})} | custom-call | flops 32212254720 | bytes 8388608 | tf_op jit(solution)/shard_map/flash/pallas_call | solution.py:391
  551.7 90.4 %mlp.5 = (bf16[256,4096]{1,0:T(8,128)(2,1)}, bf16[256,4096]{1,0:T(8,128)(2,1)}) custom-call(bf16[256,4096]{1,0:T(8,128)(2,1)} %get-tuple-element.108.refs_0_, bf16[256,4096]{1,0:T(8,128)(2,1)} %collective-permute-done.29.refs_1_, bf16[4096,3072]{1,0:T(8,128)(2,1)} %refs_2_.9, bf16[4096,3072]{1,0:T(8,128)(2,1)} %refs_3_.9, bf16[3072,4096]{1,0:T(8,128)(2,1)} %refs_4_.9, ...), custom_call_target="tpu_custom_call" | custom-call | flops 77309411328 | bytes 75497472 | tf_op jit(solution)/shard_map/mlp/pallas_call | solution.py:663
  642.1 29.0 %outp.3 = (bf16[256,4096]{1,0:T(8,128)(2,1)}, bf16[256,4096]{1,0:T(8,128)(2,1)}, bf16[256,4096]{1,0:T(8,128)(2,1)}, bf16[256,4096]{1,0:T(8,128)(2,1)}) custom-call(bf16[2,256,1024]{2,1,0:T(8,128)(2,1)} %get-tuple-element.118.refs_0_, bf16[2,256,1024]{2,1,0:T(8,128)(2,1)} %collective-permute-done.32.refs_1_, ...), custom_call_target="tpu_custom_call" | custom-call | flops 17179869184 | bytes 33554432 | tf_op jit(solution)/shard_map/outp/pallas_call | solution.py:502
  671.1 2.2 collective-permute-start.36
  675.3 90.6 %mlp.6 = (bf16[256,4096]{1,0:T(8,128)(2,1)}, bf16[256,4096]{1,0:T(8,128)(2,1)}) custom-call(bf16[256,4096]{1,0:T(8,128)(2,1)} %get-tuple-element.117.refs_0_, bf16[256,4096]{1,0:T(8,128)(2,1)} %collective-permute-done.31.refs_1_, bf16[4096,3072]{1,0:T(8,128)(2,1)} %refs_2_.9, bf16[4096,3072]{1,0:T(8,128)(2,1)} %refs_3_.9, bf16[3072,4096]{1,0:T(8,128)(2,1)} %refs_4_.9, ...), custom_call_target="tpu_custom_call" | custom-call | flops 77309411328 | bytes 75497472 | tf_op jit(solution)/shard_map/mlp/pallas_call | solution.py:663
  766.0 44.0 %collective-permute-done.30.refs_1_ = bf16[256,4096]{1,0:T(8,128)(2,1)} collective-permute-done((bf16[256,4096]{1,0:T(8,128)(2,1)}, bf16[256,4096]{1,0:T(8,128)(2,1)}, u32[]{:S(2)}, u32[]{:S(2)}) %collective-permute-start.30) | collective-permute-done | bytes 2097184 | tf_op jit(solution)/shard_map/ppermute | solution.py:803
  810.0 4.9 zsum.5.refs_5_.refs_0_
  814.9 90.5 %mlp.7 = (bf16[256,4096]{1,0:T(8,128)(2,1)}, bf16[256,4096]{1,0:T(8,128)(2,1)}) custom-call(bf16[256,4096]{1,0:T(8,128)(2,1)} %get-tuple-element.126.refs_0_, bf16[256,4096]{1,0:T(8,128)(2,1)} %collective-permute-done.36.refs_1_, bf16[4096,3072]{1,0:T(8,128)(2,1)} %refs_2_.9, bf16[4096,3072]{1,0:T(8,128)(2,1)} %refs_3_.9, bf16[3072,4096]{1,0:T(8,128)(2,1)} %refs_4_.9, ...), custom_call_target="tpu_custom_call" | custom-call | flops 77309411328 | bytes 75497472 | tf_op jit(solution)/shard_map/mlp/pallas_call | solution.py:663
  905.4 2.0 collective-permute-start.37
  907.4 4.9 zsum.6.refs_5_.refs_0_
  912.4 49.7 %mlp.8 = (bf16[128,4096]{1,0:T(8,128)(2,1)}, bf16[128,4096]{1,0:T(8,128)(2,1)}) custom-call(bf16[256,4096]{1,0:T(8,128)(2,1)} %get-tuple-element.129.refs_0_, bf16[256,4096]{1,0:T(8,128)(2,1)} %collective-permute-done.38.refs_1_, bf16[4096,3072]{1,0:T(8,128)(2,1)} %refs_2_.9, bf16[4096,3072]{1,0:T(8,128)(2,1)} %refs_3_.9, bf16[3072,4096]{1,0:T(8,128)(2,1)} %refs_4_.9, ...), custom_call_target="tpu_custom_call" | custom-call | flops 38654705664 | bytes 75497472 | tf_op jit(solution)/shard_map/mlp/pallas_call | solution.py:663
  962.4 4.9 zsum.7.refs_5_.refs_0_
  967.3 61.8 %mlp.9.refs_4_.refs_1_ = bf16[128,4096]{1,0:T(8,128)(2,1)} custom-call(bf16[256,4096]{1,0:T(8,128)(2,1)} %get-tuple-element.129.refs_0_, bf16[256,4096]{1,0:T(8,128)(2,1)} %collective-permute-done.38.refs_1_, bf16[4096,3072]{1,0:T(8,128)(2,1)} %refs_2_.9, bf16[4096,3072]{1,0:T(8,128)(2,1)} %refs_3_.9, bf16[3072,4096]{1,0:T(8,128)(2,1)} %refs_4_.9, ...), custom_call_target="tpu_custom_call" | custom-call | flops 38654705664 | bytes 75497472 | tf_op jit(solution)/shard_map/mlp/pallas_call | solution.py:663
  1029.2 2.9 zsum.8.refs_0_
  1032.0 2.4 zsum.9
  (77 shorter events, 31.0 us)
Async XLA Ops:
  4.7 68.3 %collective-permute-start.5 = (bf16[256,4096]{1,0:T(8,128)(2,1)}, bf16[256,4096]{1,0:T(8,128)(2,1)}, u32[]{:S(2)}, u32[]{:S(2)}) collective-permute-start(bf16[256,4096]{1,0:T(8,128)(2,1)} %norm.2.refs_2_.refs_0_), channel_id=1, source_target_pairs={{0,2},{1,3},{2,0},{3,1},{4,6},{5,7},{6,4},{7,5}} | collective-permute-start | bytes 6291464 | tf_op jit(solution)/shard_map/ppermute | solution.py:803
  8.0 27.3 %collective-permute-start = (bf16[256,4096]{1,0:T(8,128)(2,1)}, bf16[256,4096]{1,0:T(8,128)(2,1)}, u32[]{:S(2)}, u32[]{:S(2)}) collective-permute-start(bf16[256,4096]{1,0:T(8,128)(2,1)} %norm.2.refs_2_.refs_0_), channel_id=1, source_target_pairs={{0,1},{1,0},{2,3},{3,2},{4,5},{5,4},{6,7},{7,6}} | collective-permute-start | bytes 6291464 | tf_op jit(solution)/shard_map/ppermute | solution.py:803
  16.6 18.7 %collective-permute-start.1 = (bf16[256,4096]{1,0:T(8,128)(2,1)}, bf16[256,4096]{1,0:T(8,128)(2,1)}, u32[]{:S(2)}, u32[]{:S(2)}) collective-permute-start(bf16[256,4096]{1,0:T(8,128)(2,1)} %get-tuple-element.69.refs_1_), channel_id=1, source_target_pairs={{0,1},{1,0},{2,3},{3,2},{4,5},{5,4},{6,7},{7,6}} | collective-permute-start | bytes 6291464 | tf_op jit(solution)/shard_map/ppermute | solution.py:803
  17.1 18.2 %collective-permute-start.2 = (bf16[256,4096]{1,0:T(8,128)(2,1)}, bf16[256,4096]{1,0:T(8,128)(2,1)}, u32[]{:S(2)}, u32[]{:S(2)}) collective-permute-start(bf16[256,4096]{1,0:T(8,128)(2,1)} %get-tuple-element.70.refs_2_), channel_id=1, source_target_pairs={{0,1},{1,0},{2,3},{3,2},{4,5},{5,4},{6,7},{7,6}} | collective-permute-start | bytes 6291464 | tf_op jit(solution)/shard_map/ppermute | solution.py:803
  17.1 18.2 %collective-permute-start.3 = (bf16[256,4096]{1,0:T(8,128)(2,1)}, bf16[256,4096]{1,0:T(8,128)(2,1)}, u32[]{:S(2)}, u32[]{:S(2)}) collective-permute-start(bf16[256,4096]{1,0:T(8,128)(2,1)} %get-tuple-element.71.refs_3_), channel_id=1, source_target_pairs={{0,1},{1,0},{2,3},{3,2},{4,5},{5,4},{6,7},{7,6}} | collective-permute-start | bytes 6291464 | tf_op jit(solution)/shard_map/ppermute | solution.py:803
  17.7 10.9 %copy-start.2 = (f32[64]{0:T(128)}, f32[64]{0:T(128)S(1)}, u32[]{:S(2)}) copy-start(f32[64]{0:T(128)S(1)} %multiply_power_fusion) | copy-start | bytes 772
  19.1 12.3 %copy-start = (bf16[4096,2,128]{2,1,0:T(2,128)(2,1)S(1)}, bf16[4096,2,128]{2,1,0:T(2,128)(2,1)}, u32[]{:S(2)}) copy-start(bf16[4096,2,128]{2,1,0:T(2,128)(2,1)} %param.15) | copy-start | bytes 6291460
  31.3 2.0 copy-start.1
  73.0 4.5 collective-permute-start.6
  73.0 48.3 %collective-permute-start.4 = (bf16[256,4096]{1,0:T(8,128)(2,1)}, bf16[256,4096]{1,0:T(8,128)(2,1)}, u32[]{:S(2)}, u32[]{:S(2)}) collective-permute-start(bf16[256,4096]{1,0:T(8,128)(2,1)} %get-tuple-element.69.refs_1_), channel_id=1, source_target_pairs={{0,2},{1,3},{2,0},{3,1},{4,6},{5,7},{6,4},{7,5}} | collective-permute-start | bytes 6291464 | tf_op jit(solution)/shard_map/ppermute | solution.py:803
  121.4 4.5 collective-permute-start.7
  121.4 68.1 %collective-permute-start.8 = (bf16[256,4096]{1,0:T(8,128)(2,1)}, bf16[256,4096]{1,0:T(8,128)(2,1)}, u32[]{:S(2)}, u32[]{:S(2)}) collective-permute-start(bf16[256,4096]{1,0:T(8,128)(2,1)} %get-tuple-element.70.refs_2_), channel_id=1, source_target_pairs={{0,2},{1,3},{2,0},{3,1},{4,6},{5,7},{6,4},{7,5}} | collective-permute-start | bytes 6291464 | tf_op jit(solution)/shard_map/ppermute | solution.py:803
  189.5 5.1 collective-permute-start.9
  190.5 47.9 %collective-permute-start.10 = (bf16[256,4096]{1,0:T(8,128)(2,1)}, bf16[256,4096]{1,0:T(8,128)(2,1)}, u32[]{:S(2)}, u32[]{:S(2)}) collective-permute-start(bf16[256,4096]{1,0:T(8,128)(2,1)} %get-tuple-element.71.refs_3_), channel_id=1, source_target_pairs={{0,2},{1,3},{2,0},{3,1},{4,6},{5,7},{6,4},{7,5}} | collective-permute-start | bytes 6291464 | tf_op jit(solution)/shard_map/ppermute | solution.py:803
  238.4 5.4 collective-permute-start.11
  238.4 48.8 %collective-permute-start.12 = (bf16[8,2,256,256]{3,2,1,0:T(8,128)(2,1)}, bf16[8,2,256,256]{3,2,1,0:T(8,128)(2,1)}, u32[]{:S(2)}, u32[]{:S(2)}) collective-permute-start(bf16[8,2,256,256]{3,2,1,0:T(8,128)(2,1)} %get-tuple-element.77.refs_5_.refs_3_), channel_id=1, source_target_pairs={{0,4},{4,0},{1,5},{5,1},{2,6},{6,2},{3,7},{7,3}} | collective-permute-start | bytes 6291464 | tf_op jit(solution)/shard_map/ppermute | solution.py:803
  241.3 57.2 %collective-permute-start.13 = (bf16[2,2,256,256]{3,2,1,0:T(8,128)(2,1)}, bf16[2,2,256,256]{3,2,1,0:T(8,128)(2,1)}, u32[]{:S(2)}, u32[]{:S(2)}) collective-permute-start(bf16[2,2,256,256]{3,2,1,0:T(8,128)(2,1)} %get-tuple-element.80.refs_5_.refs_4_), channel_id=1, source_target_pairs={{0,4},{4,0},{1,5},{5,1},{2,6},{6,2},{3,7},{7,3}} | collective-permute-start | bytes 1572872 | tf_op jit(solution)/shard_map/ppermute | solution.py:803
  241.8 68.0 %collective-permute-start.14 = (bf16[2,2,256,256]{3,2,1,0:T(8,128)(2,1)}, bf16[2,2,256,256]{3,2,1,0:T(8,128)(2,1)}, u32[]{:S(2)}, u32[]{:S(2)}) collective-permute-start(bf16[2,2,256,256]{3,2,1,0:T(8,128)(2,1)} %get-tuple-element.83.refs_5_), channel_id=1, source_target_pairs={{0,4},{4,0},{1,5},{5,1},{2,6},{6,2},{3,7},{7,3}} | collective-permute-start | bytes 1572872 | tf_op jit(solution)/shard_map/ppermute | solution.py:803
  243.3 77.6 %collective-permute-start.15 = (bf16[2,2,256,256]{3,2,1,0:T(8,128)(2,1)}, bf16[2,2,256,256]{3,2,1,0:T(8,128)(2,1)}, u32[]{:S(2)}, u32[]{:S(2)}) collective-permute-start(bf16[2,2,256,256]{3,2,1,0:T(8,128)(2,1)} %get-tuple-element.87.refs_5_.refs_6_), channel_id=1, source_target_pairs={{0,4},{4,0},{1,5},{5,1},{2,6},{6,2},{3,7},{7,3}} | collective-permute-start | bytes 1572872 | tf_op jit(solution)/shard_map/ppermute | solution.py:803
  251.6 80.1 %collective-permute-start.16 = (bf16[2,2,256,256]{3,2,1,0:T(8,128)(2,1)}, bf16[2,2,256,256]{3,2,1,0:T(8,128)(2,1)}, u32[]{:S(2)}, u32[]{:S(2)}) collective-permute-start(bf16[2,2,256,256]{3,2,1,0:T(8,128)(2,1)} %qkv.10.refs_5_.refs_7_), channel_id=1, source_target_pairs={{0,4},{4,0},{1,5},{5,1},{2,6},{6,2},{3,7},{7,3}} | collective-permute-start | bytes 1572872 | tf_op jit(solution)/shard_map/ppermute | solution.py:803
  287.3 176.0 %collective-permute-start.20 = (bf16[1024,4096]{1,0:T(8,128)(2,1)}, bf16[1024,4096]{1,0:T(8,128)(2,1)}, u32[]{:S(2)}, u32[]{:S(2)}) collective-permute-start(bf16[1024,4096]{1,0:T(8,128)(2,1)} %bitcast.22), channel_id=1, source_target_pairs={{0,1},{1,0},{2,3},{3,2},{4,5},{5,4},{6,7},{7,6}} | collective-permute-start | bytes 25165832 | tf_op jit(solution)/shard_map/ppermute | solution.py:803
  298.5 62.4 %collective-permute-start.21 = (bf16[256,4096]{1,0:T(8,128)(2,1)}, bf16[256,4096]{1,0:T(8,128)(2,1)}, u32[]{:S(2)}, u32[]{:S(2)}) collective-permute-start(bf16[256,4096]{1,0:T(8,128)(2,1)} %get-tuple-element.99), channel_id=1, source_target_pairs={{0,2},{1,3},{2,0},{3,1},{4,6},{5,7},{6,4},{7,5}} | collective-permute-start | bytes 6291464 | tf_op jit(solution)/shard_map/ppermute | solution.py:803
  309.7 95.9 %collective-permute-start.22 = (bf16[256,4096]{1,0:T(8,128)(2,1)}, bf16[256,4096]{1,0:T(8,128)(2,1)}, u32[]{:S(2)}, u32[]{:S(2)}) collective-permute-start(bf16[256,4096]{1,0:T(8,128)(2,1)} %get-tuple-element.101), channel_id=1, source_target_pairs={{0,2},{1,3},{2,0},{3,1},{4,6},{5,7},{6,4},{7,5}} | collective-permute-start | bytes 6291464 | tf_op jit(solution)/shard_map/ppermute | solution.py:803
  360.9 47.5 %collective-permute-start.23 = (bf16[256,4096]{1,0:T(8,128)(2,1)}, bf16[256,4096]{1,0:T(8,128)(2,1)}, u32[]{:S(2)}, u32[]{:S(2)}) collective-permute-start(bf16[256,4096]{1,0:T(8,128)(2,1)} %collective-permute-done.21.refs_6_), channel_id=1, source_target_pairs={{0,4},{4,0},{1,5},{5,1},{2,6},{6,2},{3,7},{7,3}} | collective-permute-start | bytes 6291464 | tf_op jit(solution)/shard_map/ppermute | solution.py:803
  405.7 50.1 %collective-permute-start.17 = (bf16[2,256,1024]{2,1,0:T(8,128)(2,1)}, bf16[2,256,1024]{2,1,0:T(8,128)(2,1)}, u32[]{:S(2)}, u32[]{:S(2)}) collective-permute-start(bf16[2,256,1024]{2,1,0:T(8,128)(2,1)} %get-tuple-element.95), channel_id=1, source_target_pairs={{0,1},{1,0},{2,3},{3,2},{4,5},{5,4},{6,7},{7,6}} | collective-permute-start | bytes 3145736 | tf_op jit(solution)/shard_map/ppermute | solution.py:803
  405.7 50.5 %collective-permute-start.18 = (bf16[2,256,1024]{2,1,0:T(8,128)(2,1)}, bf16[2,256,1024]{2,1,0:T(8,128)(2,1)}, u32[]{:S(2)}, u32[]{:S(2)}) collective-permute-start(bf16[2,256,1024]{2,1,0:T(8,128)(2,1)} %get-tuple-element.96), channel_id=1, source_target_pairs={{0,2},{1,3},{2,0},{3,1},{4,6},{5,7},{6,4},{7,5}} | collective-permute-start | bytes 3145736 | tf_op jit(solution)/shard_map/ppermute | solution.py:803
  406.6 49.7 %collective-permute-start.19 = (bf16[2,256,1024]{2,1,0:T(8,128)(2,1)}, bf16[2,256,1024]{2,1,0:T(8,128)(2,1)}, u32[]{:S(2)}, u32[]{:S(2)}) collective-permute-start(bf16[2,256,1024]{2,1,0:T(8,128)(2,1)} %get-tuple-element.97), channel_id=1, source_target_pairs={{0,3},{1,2},{2,1},{3,0},{4,7},{5,6},{6,5},{7,4}} | collective-permute-start | bytes 3145736 | tf_op jit(solution)/shard_map/ppermute | solution.py:803
  408.4 47.3 %collective-permute-start.24 = (bf16[256,4096]{1,0:T(8,128)(2,1)}, bf16[256,4096]{1,0:T(8,128)(2,1)}, u32[]{:S(2)}, u32[]{:S(2)}) collective-permute-start(bf16[256,4096]{1,0:T(8,128)(2,1)} %collective-permute-done.22.refs_7_), channel_id=1, source_target_pairs={{0,4},{4,0},{1,5},{5,1},{2,6},{6,2},{3,7},{7,3}} | collective-permute-start | bytes 6291464 | tf_op jit(solution)/shard_map/ppermute | solution.py:803
  455.7 4.5 collective-permute-start.25
  455.7 7.5 collective-permute-start.26
  456.2 10.0 collective-permute-start.27
  456.3 13.0 %collective-permute-start.28 = (bf16[256,4096]{1,0:T(8,128)(2,1)}, bf16[256,4096]{1,0:T(8,128)(2,1)}, u32[]{:S(2)}, u32[]{:S(2)}) collective-permute-start(bf16[256,4096]{1,0:T(8,128)(2,1)} %collective-permute-done.24.refs_9_), channel_id=1, source_target_pairs={{0,1},{1,0},{2,3},{3,2},{4,5},{5,4},{6,7},{7,6}} | collective-permute-start | bytes 6291464 | tf_op jit(solution)/shard_map/ppermute | solution.py:803
  498.2 53.5 %collective-permute-start.29 = (bf16[256,4096]{1,0:T(8,128)(2,1)}, bf16[256,4096]{1,0:T(8,128)(2,1)}, u32[]{:S(2)}, u32[]{:S(2)}) collective-permute-start(bf16[256,4096]{1,0:T(8,128)(2,1)} %get-tuple-element.108.refs_0_), channel_id=1, source_target_pairs={{0,2},{1,3},{2,0},{3,1},{4,6},{5,7},{6,4},{7,5}} | collective-permute-start | bytes 6291464 | tf_op jit(solution)/shard_map/ppermute | solution.py:803
  549.3 92.8 %collective-permute-start.32 = (bf16[2,256,1024]{2,1,0:T(8,128)(2,1)}, bf16[2,256,1024]{2,1,0:T(8,128)(2,1)}, u32[]{:S(2)}, u32[]{:S(2)}) collective-permute-start(bf16[2,256,1024]{2,1,0:T(8,128)(2,1)} %get-tuple-element.119), channel_id=1, source_target_pairs={{0,1},{1,0},{2,3},{3,2},{4,5},{5,4},{6,7},{7,6}} | collective-permute-start | bytes 3145736 | tf_op jit(solution)/shard_map/ppermute | solution.py:803
  549.3 92.8 %collective-permute-start.33 = (bf16[2,256,1024]{2,1,0:T(8,128)(2,1)}, bf16[2,256,1024]{2,1,0:T(8,128)(2,1)}, u32[]{:S(2)}, u32[]{:S(2)}) collective-permute-start(bf16[2,256,1024]{2,1,0:T(8,128)(2,1)} %get-tuple-element.120), channel_id=1, source_target_pairs={{0,2},{1,3},{2,0},{3,1},{4,6},{5,7},{6,4},{7,5}} | collective-permute-start | bytes 3145736 | tf_op jit(solution)/shard_map/ppermute | solution.py:803
  549.4 92.7 %collective-permute-start.34 = (bf16[2,256,1024]{2,1,0:T(8,128)(2,1)}, bf16[2,256,1024]{2,1,0:T(8,128)(2,1)}, u32[]{:S(2)}, u32[]{:S(2)}) collective-permute-start(bf16[2,256,1024]{2,1,0:T(8,128)(2,1)} %get-tuple-element.121), channel_id=1, source_target_pairs={{0,3},{1,2},{2,1},{3,0},{4,7},{5,6},{6,5},{7,4}} | collective-permute-start | bytes 3145736 | tf_op jit(solution)/shard_map/ppermute | solution.py:803
  551.2 124.1 %collective-permute-start.31 = (bf16[256,4096]{1,0:T(8,128)(2,1)}, bf16[256,4096]{1,0:T(8,128)(2,1)}, u32[]{:S(2)}, u32[]{:S(2)}) collective-permute-start(bf16[256,4096]{1,0:T(8,128)(2,1)} %get-tuple-element.117.refs_0_), channel_id=1, source_target_pairs={{0,2},{1,3},{2,0},{3,1},{4,6},{5,7},{6,4},{7,5}} | collective-permute-start | bytes 6291464 | tf_op jit(solution)/shard_map/ppermute | solution.py:803
  671.1 143.8 %collective-permute-start.36 = (bf16[256,4096]{1,0:T(8,128)(2,1)}, bf16[256,4096]{1,0:T(8,128)(2,1)}, u32[]{:S(2)}, u32[]{:S(2)}) collective-permute-start(bf16[256,4096]{1,0:T(8,128)(2,1)} %get-tuple-element.126.refs_0_), channel_id=1, source_target_pairs={{0,2},{1,3},{2,0},{3,1},{4,6},{5,7},{6,4},{7,5}} | collective-permute-start | bytes 6291464 | tf_op jit(solution)/shard_map/ppermute | solution.py:803
  673.3 239.1 %collective-permute-start.38 = (bf16[256,4096]{1,0:T(8,128)(2,1)}, bf16[256,4096]{1,0:T(8,128)(2,1)}, u32[]{:S(2)}, u32[]{:S(2)}) collective-permute-start(bf16[256,4096]{1,0:T(8,128)(2,1)} %get-tuple-element.129.refs_0_), channel_id=1, source_target_pairs={{0,2},{1,3},{2,0},{3,1},{4,6},{5,7},{6,4},{7,5}} | collective-permute-start | bytes 6291464 | tf_op jit(solution)/shard_map/ppermute | solution.py:803
  673.3 136.6 %collective-permute-start.30 = (bf16[256,4096]{1,0:T(8,128)(2,1)}, bf16[256,4096]{1,0:T(8,128)(2,1)}, u32[]{:S(2)}, u32[]{:S(2)}) collective-permute-start(bf16[256,4096]{1,0:T(8,128)(2,1)} %get-tuple-element.116), channel_id=1, source_target_pairs={{0,2},{1,3},{2,0},{3,1},{4,6},{5,7},{6,4},{7,5}} | collective-permute-start | bytes 6291464 | tf_op jit(solution)/shard_map/ppermute | solution.py:803
  765.9 141.5 %collective-permute-start.35 = (bf16[256,4096]{1,0:T(8,128)(2,1)}, bf16[256,4096]{1,0:T(8,128)(2,1)}, u32[]{:S(2)}, u32[]{:S(2)}) collective-permute-start(bf16[256,4096]{1,0:T(8,128)(2,1)} %get-tuple-element.124), channel_id=1, source_target_pairs={{0,2},{1,3},{2,0},{3,1},{4,6},{5,7},{6,4},{7,5}} | collective-permute-start | bytes 6291464 | tf_op jit(solution)/shard_map/ppermute | solution.py:803
  905.4 57.0 %collective-permute-start.37 = (bf16[256,4096]{1,0:T(8,128)(2,1)}, bf16[256,4096]{1,0:T(8,128)(2,1)}, u32[]{:S(2)}, u32[]{:S(2)}) collective-permute-start(bf16[256,4096]{1,0:T(8,128)(2,1)} %get-tuple-element.128), channel_id=1, source_target_pairs={{0,2},{1,3},{2,0},{3,1},{4,6},{5,7},{6,4},{7,5}} | collective-permute-start | bytes 6291464 | tf_op jit(solution)/shard_map/ppermute | solution.py:803
  962.0 67.1 %collective-permute-start.39 = (bf16[128,4096]{1,0:T(8,128)(2,1)}, bf16[128,4096]{1,0:T(8,128)(2,1)}, u32[]{:S(2)}, u32[]{:S(2)}) collective-permute-start(bf16[128,4096]{1,0:T(8,128)(2,1)} %get-tuple-element.131), channel_id=1, source_target_pairs={{0,2},{1,3},{2,0},{3,1},{4,6},{5,7},{6,4},{7,5}} | collective-permute-start | bytes 3145736 | tf_op jit(solution)/shard_map/ppermute | solution.py:803

commit v16 on v15

--- a/solution.py
+++ b/solution.py
@@ -21,6 +21,7 @@
 
 
 VMEM = 67043328
+PAIR = (0, 1)
 PARAMS = pltpu.CompilerParams(vmem_limit_bytes=VMEM)
 
 
@@ -35,6 +36,11 @@
     f = rows.astype(F32)
     mean_sq = jnp.mean(f * f, axis=-1, keepdims=True)
     return (f * lax.rsqrt(mean_sq + NORM_EPS) * gain.astype(F32)).astype(BF)
+
+
+def other_core():
+    me = lax.axis_index('tp')
+    return {'tp': me + 1 - 2 * lax.rem(me, 2)}
 
 
 def cost(flops, moved):
@@ -119,12 +125,13 @@
     lax.fori_loop(0, n_in // group, one, 0)
 
 
-def qkv(rows, w_all, tables, with_q=True, with_kv=True, after=(), group=2):
+def qkv(rows, w_all, tables, with_q=True, with_kv=True, after=()):
     n_in = len(rows)
     dim = w_all.shape[0]
     tn = 512
     n_q = w_all.shape[1] // tn - 1
     (cos, sin), first_run = tables
+    group = 2
     at = first_run // n_in
     start = 0 if with_q else n_q
     kv_shape = (n_in, 2, RUN, RUN)
@@ -417,14 +424,18 @@
     )(tab, *qs, *kvs, *sts, *more, *after)
 
 
-def out_kernel(*refs, blocks, n_w, n_run, at):
+def out_kernel(*refs, blocks, n_w, n_run, at, n_shared):
     n_o, n_out = 4, 2 * n_run
     o_refs, w_refs, x_ref, g_ref = refs[:n_o], refs[n_o:n_o + n_w], refs[n_o + n_w], refs[n_o + n_w + 1]
     outs = refs[n_o + n_w + 2:n_o + n_w + 2 + n_out]
-    o_scr, w_scr, x_scr, acc_scr, o_sem, w_sem, x_sem, out_sem = refs[n_o + n_w + 2 + n_out:]
+    o_scr, w_scr, x_scr, acc_scr, o_sem, w_sem, x_sem, out_sem, sent_sem = refs[n_o + n_w + 2 + n_out:]
     width = o_refs[0].shape[-1]
     half = width // 2
-    n_slots = w_scr.shape[0]
+    n_slots = w_scr.shape[0] - n_shared
+    n_local = len(blocks)
+    mate = other_core()
+    barrier = pltpu.get_barrier_semaphore()
+    pl.semaphore_signal(barrier, inc=1, device_id=mate, device_id_type=pl.DeviceIdType.MESH)
 
     def fetch(k):
         for i, pieces in enumerate(blocks):
@@ -437,7 +448,7 @@
                     to += n
 
     mine = lax.axis_index('cp')
-    loads = [[] for _ in blocks]
+    loads = [[] for _ in range(n_local + n_shared)]
     for i in range(n_run):
         rows = pl.ds(i * RUN, RUN)
         for k in range(4):
@@ -454,6 +465,17 @@
         cp.start()
     for i in range(n_slots - 1):
         fetch(jnp.int32(i))
+    shared = []
+    pl.semaphore_wait(barrier, 1)
+    for b in range(n_shared):
+        to = 0
+        for a, r0, n in blocks[b - n_shared]:
+            shared.append(pltpu.make_async_remote_copy(
+                src_ref=w_refs[a].at[pl.ds(r0, n), :], dst_ref=w_scr.at[n_slots + b, pl.ds(to, n), :],
+                send_sem=sent_sem.at[len(shared)], recv_sem=w_sem.at[n_slots + b], device_id=mate,
+                device_id_type=pl.DeviceIdType.MESH))
+            shared[-1].start()
+            to += n
     for ls in copies[1:]:
         for cp in ls:
             cp.start()
@@ -468,12 +490,12 @@
                 def _():
                     for cp in ls:
                         cp.wait()
-        slot = lax.rem(k, n_slots)
+        slot = jnp.where(k < n_local, lax.rem(k, n_slots), k - n_local + n_slots)
         pltpu.make_async_copy(w_scr.at[slot], w_scr.at[slot], w_sem.at[slot]).wait()
         acc_scr[:] += jnp.dot(o_scr[:, pl.ds(pl.multiple_of(k * half, half), half)], w_scr[slot], preferred_element_type=F32)
         return carry
 
-    lax.fori_loop(0, len(blocks), one, 0)
+    lax.fori_loop(0, len(loads), one, 0)
     x_copy.wait()
 
     strip = 32
@@ -493,23 +515,27 @@
             stores[-1].start()
     for cp in stores:
         cp.wait()
-
-
-def out_proj(os, ws, blocks, x_rows, gain, at, after=()):
+    for cp in shared:
+        cp.wait_send()
+
+
+def out_proj(os, ws, blocks, n_shared, x_rows, gain, at, call, after=()):
     dim = x_rows.shape[1]
     n_run, _, width = os[0].shape
     rows = n_run * RUN
     return pl.pallas_call(
-        ordered(functools.partial(out_kernel, blocks=blocks, n_w=len(ws), n_run=n_run, at=at),
+        ordered(functools.partial(out_kernel, blocks=blocks, n_w=len(ws), n_run=n_run, at=at, n_shared=n_shared),
                 len(os) + len(ws) + 2, after),
         grid=(1,),
         in_specs=[ANY] * (len(os) + len(ws) + 1) + [pl.BlockSpec((1, dim), lambda i: (0, 0))] + [ANY] * len(after),
         out_specs=[ANY] * (2 * n_run),
         out_shape=[jax.ShapeDtypeStruct((RUN, dim), BF)] * (2 * n_run),
-        scratch_shapes=[pltpu.VMEM((rows, 4 * width), BF), pltpu.VMEM((3, width // 2, dim), BF), pltpu.VMEM((rows, dim), BF),
-                        pltpu.VMEM((rows, dim), F32), pltpu.SemaphoreType.DMA((len(blocks), 2 * n_run)),
-                        pltpu.SemaphoreType.DMA((3,)), pltpu.SemaphoreType.DMA, pltpu.SemaphoreType.DMA((2 * n_run,))],
-        name="outp", compiler_params=PARAMS,
+        scratch_shapes=[pltpu.VMEM((rows, 4 * width), BF), pltpu.VMEM((3 + n_shared, width // 2, dim), BF), pltpu.VMEM((rows, dim), BF),
+                        pltpu.VMEM((rows, dim), F32), pltpu.SemaphoreType.DMA((len(blocks) + n_shared, 2 * n_run)),
+                        pltpu.SemaphoreType.DMA((3 + n_shared,)), pltpu.SemaphoreType.DMA, pltpu.SemaphoreType.DMA((2 * n_run,)),
+                        pltpu.SemaphoreType.DMA((len(ws),))],
+        name="outp",
+        compiler_params=pltpu.CompilerParams(vmem_limit_bytes=VMEM, collective_id=call, has_side_effects=True),
         cost_estimate=cost(8 * rows * width * dim, 8 * width * dim),
     )(*os, *ws, x_rows, gain, *after)
 
@@ -520,13 +546,12 @@
     (b_scr, u_scr, w_scr, d_scr, keep_scr, out_scr, in_scr, b_sem, w_sem, d_sem, out_sem, in_sem,
      rows_sem, *more) = refs[n_in + (4 if cross else 5):]
     i = pl.program_id(0)
-    me = lax.axis_index('tp')
-    mate = {'tp': me + 1 - 2 * lax.rem(me, 2)}
+    mate = other_core()
     peers = [mate]
     if cross:
         own_scr, far_scr, back_scr, far_sem, back_sem = more
         half_tp = lax.axis_size('tp') // 2
-        peers.append({'tp': lax.rem(me + half_tp, 2 * half_tp)})
+        peers.append({'tp': lax.rem(lax.axis_index('tp') + half_tp, 2 * half_tp)})
     barrier = pltpu.get_barrier_semaphore()
 
     def fetch(j):
@@ -836,7 +861,7 @@
         rows = half // n_piece
         wo_c = send(over_core, tied(wo, kvs[-1]))
 
-        tiles = [(0, i) for i in range(2 * n_run)] + [(1, i) for i in (0, 1)]
+        tiles = [(0, i) for i in range(2 * n_run)] + [(1, i) for i in PAIR]
         st, *wo_x = flash(tab, [q_here, q_far[0]], tiles, kvs, base=bases[0], work=int(work[0]), cut=wo,
                          n_cut=n_piece)
         wo_x = [send(over_x, w) for w in wo_x]
@@ -844,16 +869,11 @@
         kvs = kvs + [send(over_y, kv) for kv in kvs]
 
         os, outs, prev = [], [], q_far[-1]
-        wo_a, wo_ya, wo_yb = {}, {}, {}
+        wo_a, wo_b = [], []
 
         def forward_w(p):
-            here = tied(wo_x[p], prev)
-            wo_ya[p] = (here, send(over_core, here))
-            wo_a[p] = send(over_y, here)
-
-        def relay_w(p):
-            here = tied(wo_a[p], prev)
-            wo_yb[p] = (here, send(over_core, here))
+            wo_a.append(tied(wo_x[p], prev))
+            wo_b.append(send(over_y, wo_a[p]))
 
         def attend(j):
             held = 2 * n_run + 2 * j
@@ -869,13 +889,10 @@
             return done
 
         def project(i):
-            ws = [wo, wo_c]
-            blocks = [[(a, r, half)] for a in (0, 1) for r in (0, half)]
-            for k in range(2):
-                for held in (wo_ya, wo_yb):
-                    blocks.append([(len(ws) + p, 0, rows) for p in range(n_piece)])
-                    ws += [held[p][k] for p in range(n_piece)]
-            got = out_proj(os[i], ws, blocks, x_rows, gm, i, after=(prev,))
+            ws = [wo, wo_c, *wo_a, *wo_b]
+            blocks = [[(a, r, half)] for a in PAIR for r in (0, half)]
+            blocks += [[(2 + b * n_piece + p, 0, rows) for p in range(n_piece)] for b in PAIR]
+            got = out_proj(os[i], ws, blocks, 2, x_rows, gm, i, n_run + 1 + i, after=(prev,))
             for y, b in zip(got[::2], got[1::2]):
                 outs.append((y, b, send(over_x, b)))
             return got[0]
@@ -885,8 +902,6 @@
             prev = attend(j)
             if j < n_piece:
                 forward_w(j)
-            if j:
-                relay_w(j - 1)
         prev = project(0)
         prev = attend(last)
 

time: 1040 us -> 1070 us (1.029)
  waiting for transfers between devices: 191 us -> 223 us
    ppermute x40 -> x36, waiting for transfers between devices: 191 us -> 223 us  [send(): return lax.ppermute(v, *axis_pairs)]
    ppermute x40 -> x36, starting transfers between devices: 36.3 us -> 28.2 us  [send(): return lax.ppermute(v, *axis_pairs)]
  transfers between devices with their start and end apart: 40 -> 36, of which waited for: 18 -> 15; matrix products, arithmetic and copies ran while one was open for 2% -> 2% of each run, Pallas kernels for 72% -> 70%
where the time goes in v16:
time: 1070 us; the launch traced here: 1060 us
  Pallas kernels  780 us (73%)
  waiting for transfers between devices  223 us (21%)
  starting transfers between devices  28.2 us (3%)
  local copies, waits for them, and re-layouts  18.8 us (2%)
    pallas_call x5, Pallas kernels, mlp(): pl.pallas_call(ordered(functools.partial(mlp_kernel, n_in=len(bs), first=...  383 us
    ppermute x36, waiting for transfers between devices, send(): return lax.ppermute(v, *axis_pairs)  223 us
    pallas_call x5, Pallas kernels, flash(): pl.pallas_call(ordered(functools.partial(flash_kernel, q_src=q_src, kv_sr...  211 us
    pallas_call x6, Pallas kernels, qkv(): pl.pallas_call(ordered(functools.partial(qkv_kernel, n_in=n_in, n_q=n_q,...  97.6 us
    pallas_call x2, Pallas kernels, out_proj(): pl.pallas_call(ordered(functools.partial(out_kernel, blocks=blocks, n_w=l...  56.5 us
    ppermute x36, starting transfers between devices, send(): return lax.ppermute(v, *axis_pairs)  28.2 us
  transfers between devices with their start and end apart: 36, of which 15 were waited for; matrix products, arithmetic and copies ran while one was open for 2% of the time, Pallas kernels for 70%

profile of v16, /device:TPU:0, one launch (start us, length us, event | category | flops | bytes accessed | tf_op | source)
XLA Modules:
  0.0 1057.7 jit_solution(7960353216541394325)
XLA Ops:
  1.3 3.4 norm.2.refs_2_.refs_0_
  4.7 3.3 collective-permute-start.5
  8.0 8.6 norm.3
  19.1 9.5 bitcast_dynamic-update-slice_fusion
  28.6 2.8 multiply_sine_fusion.1
  31.4 2.0 bitcast_dynamic-update-slice_fusion.2
  33.4 2.0 bitcast_dynamic-update-slice_fusion.1.refs_8_.refs_2_
  35.4 37.6 %qkv.6 = (bf16[8,1024,256]{2,1,0:T(8,128)(2,1)}, bf16[8,2,256,256]{3,2,1,0:T(8,128)(2,1)}) custom-call(bf16[256,4096]{1,0:T(8,128)(2,1)} %norm.2.refs_2_.refs_0_, bf16[256,4096]{1,0:T(8,128)(2,1)} %get-tuple-element.67.refs_1_, bf16[256,4096]{1,0:T(8,128)(2,1)} %get-tuple-element.68.refs_2_, bf16[256,4096]{1,0:T(8,128)(2,1)} %get-tuple-element.69.refs_3_, ...), custom_call_target="tpu_custom_call" | custom-call | flops 25769803776 | bytes 12582912 | tf_op jit(solution)/shard_map/qkv/pallas_call | solution.py:139
  73.8 3.4 multiply_sine_fusion
  77.6 14.0 %qkv.7 = (bf16[2,1024,256]{2,1,0:T(8,128)(2,1)}, bf16[2,2,256,256]{3,2,1,0:T(8,128)(2,1)}) custom-call(bf16[256,4096]{1,0:T(8,128)(2,1)} %collective-permute-done.5.refs_0_, bf16[256,4096]{1,0:T(8,128)(2,1)} %collective-permute-done.6.refs_1_, bf16[4096,1536]{1,0:T(8,128)(2,1)} %bitcast_dynamic-update-slice_fusion.1.refs_8_.refs_2_, ...), custom_call_target="tpu_custom_call" | custom-call | flops 6442450944 | bytes 12582912 | tf_op jit(solution)/shard_map/qkv/pallas_call | solution.py:139
  91.6 29.8 %collective-permute-done.4.refs_0_ = bf16[256,4096]{1,0:T(8,128)(2,1)} collective-permute-done((bf16[256,4096]{1,0:T(8,128)(2,1)}, bf16[256,4096]{1,0:T(8,128)(2,1)}, u32[]{:S(2)}, u32[]{:S(2)}) %collective-permute-start.4) | collective-permute-done | bytes 2097184 | tf_op jit(solution)/shard_map/ppermute | solution.py:828
  123.1 2.9 collective-permute-done.7.refs_1_
  126.0 13.6 %qkv.8 = (bf16[2,1024,256]{2,1,0:T(8,128)(2,1)}, bf16[2,2,256,256]{3,2,1,0:T(8,128)(2,1)}) custom-call(bf16[256,4096]{1,0:T(8,128)(2,1)} %collective-permute-done.4.refs_0_, bf16[256,4096]{1,0:T(8,128)(2,1)} %collective-permute-done.7.refs_1_, bf16[4096,1536]{1,0:T(8,128)(2,1)} %bitcast_dynamic-update-slice_fusion.1.refs_8_.refs_2_, ...), custom_call_target="tpu_custom_call" | custom-call | flops 6442450944 | bytes 12582912 | tf_op jit(solution)/shard_map/qkv/pallas_call | solution.py:139
  139.5 50.0 %flash_part.1 = (f32[10,2,4,144,256]{4,3,2,1,0:T(8,128)}, bf16[256,4096]{1,0:T(8,128)(2,1)}, bf16[256,4096]{1,0:T(8,128)(2,1)}) custom-call(s32[845]{0:T(1024)} %dynamic-slice_reduce_fusion.refs_0_, bf16[8,1024,256]{2,1,0:T(8,128)(2,1)} %get-tuple-element.74.refs_1_, bf16[2,1024,256]{2,1,0:T(8,128)(2,1)} %get-tuple-element.82.refs_2_, ...), custom_call_target="tpu_custom_call" | custom-call | flops 38654705664 | bytes 3145728 | tf_op jit(solution)/shard_map/flash_part/pallas_call | solution.py:398
  191.7 3.0 collective-permute-done.9.refs_1_
  194.7 13.7 %qkv.9 = (bf16[2,1024,256]{2,1,0:T(8,128)(2,1)}, bf16[2,2,256,256]{3,2,1,0:T(8,128)(2,1)}) custom-call(bf16[256,4096]{1,0:T(8,128)(2,1)} %collective-permute-done.8.refs_0_, bf16[256,4096]{1,0:T(8,128)(2,1)} %collective-permute-done.9.refs_1_, bf16[4096,1536]{1,0:T(8,128)(2,1)} %bitcast_dynamic-update-slice_fusion.1.refs_8_.refs_2_, ...), custom_call_target="tpu_custom_call" | custom-call | flops 6442450944 | bytes 12582912 | tf_op jit(solution)/shard_map/qkv/pallas_call | solution.py:139
  208.5 30.0 %collective-permute-done.10.refs_0_ = bf16[256,4096]{1,0:T(8,128)(2,1)} collective-permute-done((bf16[256,4096]{1,0:T(8,128)(2,1)}, bf16[256,4096]{1,0:T(8,128)(2,1)}, u32[]{:S(2)}, u32[]{:S(2)}) %collective-permute-start.10) | collective-permute-done | bytes 2097184 | tf_op jit(solution)/shard_map/ppermute | solution.py:828
  243.8 7.8 qkv.10.refs_5_.refs_7_
  253.2 10.8 %qkv.11.refs_14_.refs_2_ = bf16[2,1024,256]{2,1,0:T(8,128)(2,1)} custom-call(bf16[256,4096]{1,0:T(8,128)(2,1)} %collective-permute-done.10.refs_0_, bf16[256,4096]{1,0:T(8,128)(2,1)} %collective-permute-done.11.refs_1_, bf16[4096,1536]{1,0:T(8,128)(2,1)} %bitcast_dynamic-update-slice_fusion.1.refs_8_.refs_2_, f32[8,64,256]{2,1,0:T(8,128)} %get-tuple-element.132.refs_3_, ...), custom_call_target="tpu_custom_call" | custom-call | flops 6442450944 | bytes 12582912 | tf_op jit(solution)/shard_map/qkv/pallas_call | solution.py:139
  264.0 23.3 %collective-permute-done.12.refs_8_ = bf16[8,2,256,256]{3,2,1,0:T(8,128)(2,1)} collective-permute-done((bf16[8,2,256,256]{3,2,1,0:T(8,128)(2,1)}, bf16[8,2,256,256]{3,2,1,0:T(8,128)(2,1)}, u32[]{:S(2)}, u32[]{:S(2)}) %collective-permute-start.12) | collective-permute-done | bytes 2097184 | tf_op jit(solution)/shard_map/ppermute | solution.py:828
  287.3 11.2 %collective-permute-done.13.refs_9_ = bf16[2,2,256,256]{3,2,1,0:T(8,128)(2,1)} collective-permute-done((bf16[2,2,256,256]{3,2,1,0:T(8,128)(2,1)}, bf16[2,2,256,256]{3,2,1,0:T(8,128)(2,1)}, u32[]{:S(2)}, u32[]{:S(2)}) %collective-permute-start.13) | collective-permute-done | bytes 524320 | tf_op jit(solution)/shard_map/ppermute | solution.py:828
  300.1 9.7 collective-permute-done.14.refs_10_
  311.3 9.7 collective-permute-done.15.refs_11_
  321.0 10.8 %collective-permute-done.16.refs_12_ = bf16[2,2,256,256]{3,2,1,0:T(8,128)(2,1)} collective-permute-done((bf16[2,2,256,256]{3,2,1,0:T(8,128)(2,1)}, bf16[2,2,256,256]{3,2,1,0:T(8,128)(2,1)}, u32[]{:S(2)}, u32[]{:S(2)}) %collective-permute-start.16) | collective-permute-done | bytes 524320 | tf_op jit(solution)/shard_map/ppermute | solution.py:828
  331.8 29.1 %flash.4 = (bf16[2,256,1024]{2,1,0:T(8,128)(2,1)}, bf16[2,256,1024]{2,1,0:T(8,128)(2,1)}, bf16[2,256,1024]{2,1,0:T(8,128)(2,1)}, bf16[2,256,1024]{2,1,0:T(8,128)(2,1)}, f32[8,128]{1,0:T(8,128)}) custom-call(s32[845]{0:T(1024)} %dynamic-slice_reduce_fusion.refs_0_, bf16[8,1024,256]{2,1,0:T(8,128)(2,1)} %get-tuple-element.74.refs_1_, ...), custom_call_target="tpu_custom_call" | custom-call | flops 23622320128 | bytes 8388608 | tf_op jit(solution)/shard_map/flash/pallas_call | solution.py:398
  360.9 43.9 %flash.5 = (bf16[2,256,1024]{2,1,0:T(8,128)(2,1)}, bf16[2,256,1024]{2,1,0:T(8,128)(2,1)}, bf16[2,256,1024]{2,1,0:T(8,128)(2,1)}, bf16[2,256,1024]{2,1,0:T(8,128)(2,1)}, f32[8,128]{1,0:T(8,128)}) custom-call(s32[845]{0:T(1024)} %dynamic-slice_reduce_fusion.refs_0_, ...), custom_call_target="tpu_custom_call", output_to_operand_aliasing={{0}: (14, {}), {1}: (15, {}), {2}: (16, {}), {3}: (17, {})} | custom-call | flops 32212254720 | bytes 8388608 | tf_op jit(solution)/shard_map/flash/pallas_call | solution.py:398
  404.9 1.7 collective-permute-start.18
  408.7 43.8 %flash.6 = (bf16[2,256,1024]{2,1,0:T(8,128)(2,1)}, bf16[2,256,1024]{2,1,0:T(8,128)(2,1)}, bf16[2,256,1024]{2,1,0:T(8,128)(2,1)}, bf16[2,256,1024]{2,1,0:T(8,128)(2,1)}, f32[8,128]{1,0:T(8,128)}) custom-call(s32[845]{0:T(1024)} %dynamic-slice_reduce_fusion.refs_0_, bf16[8,1024,256]{2,1,0:T(8,128)(2,1)} %get-tuple-element.74.refs_1_, ...), custom_call_target="tpu_custom_call" | custom-call | flops 32212254720 | bytes 8388608 | tf_op jit(solution)/shard_map/flash/pallas_call | solution.py:398
  452.7 2.8 collective-permute-done.23.refs_8_
  455.5 44.3 %collective-permute-done.24.refs_9_ = bf16[256,4096]{1,0:T(8,128)(2,1)} collective-permute-done((bf16[256,4096]{1,0:T(8,128)(2,1)}, bf16[256,4096]{1,0:T(8,128)(2,1)}, u32[]{:S(2)}, u32[]{:S(2)}) %collective-permute-start.24) | collective-permute-done | bytes 2097184 | tf_op jit(solution)/shard_map/ppermute | solution.py:828
  499.8 28.2 %outp.2 = (bf16[256,4096]{1,0:T(8,128)(2,1)}, bf16[256,4096]{1,0:T(8,128)(2,1)}, bf16[256,4096]{1,0:T(8,128)(2,1)}, bf16[256,4096]{1,0:T(8,128)(2,1)}) custom-call(bf16[2,256,1024]{2,1,0:T(8,128)(2,1)} %get-tuple-element.92.refs_0_, bf16[2,256,1024]{2,1,0:T(8,128)(2,1)} %collective-permute-done.17.refs_1_, ...), custom_call_target="tpu_custom_call" | custom-call | flops 17179869184 | bytes 33554432 | tf_op jit(solution)/shard_map/outp/pallas_call | solution.py:526
  529.7 43.9 %flash.7 = (bf16[2,256,1024]{2,1,0:T(8,128)(2,1)}, bf16[2,256,1024]{2,1,0:T(8,128)(2,1)}, bf16[2,256,1024]{2,1,0:T(8,128)(2,1)}, bf16[2,256,1024]{2,1,0:T(8,128)(2,1)}, f32[8,128]{1,0:T(8,128)}) custom-call(s32[845]{0:T(1024)} %dynamic-slice_reduce_fusion.refs_0_, ...), custom_call_target="tpu_custom_call", output_to_operand_aliasing={{0}: (14, {}), {1}: (15, {}), {2}: (16, {}), {3}: (17, {})} | custom-call | flops 32212254720 | bytes 8388608 | tf_op jit(solution)/shard_map/flash/pallas_call | solution.py:398
  573.6 1.8 collective-permute-start.30
  575.7 90.4 %mlp.5 = (bf16[256,4096]{1,0:T(8,128)(2,1)}, bf16[256,4096]{1,0:T(8,128)(2,1)}) custom-call(bf16[256,4096]{1,0:T(8,128)(2,1)} %get-tuple-element.104.refs_0_, bf16[256,4096]{1,0:T(8,128)(2,1)} %collective-permute-done.25.refs_1_, bf16[4096,3072]{1,0:T(8,128)(2,1)} %refs_2_.9, bf16[4096,3072]{1,0:T(8,128)(2,1)} %refs_3_.9, bf16[3072,4096]{1,0:T(8,128)(2,1)} %refs_4_.9, ...), custom_call_target="tpu_custom_call" | custom-call | flops 77309411328 | bytes 75497472 | tf_op jit(solution)/shard_map/mlp/pallas_call | solution.py:688
  666.2 28.3 %outp.3 = (bf16[256,4096]{1,0:T(8,128)(2,1)}, bf16[256,4096]{1,0:T(8,128)(2,1)}, bf16[256,4096]{1,0:T(8,128)(2,1)}, bf16[256,4096]{1,0:T(8,128)(2,1)}) custom-call(bf16[2,256,1024]{2,1,0:T(8,128)(2,1)} %get-tuple-element.114.refs_0_, bf16[2,256,1024]{2,1,0:T(8,128)(2,1)} %collective-permute-done.28.refs_1_, ...), custom_call_target="tpu_custom_call" | custom-call | flops 17179869184 | bytes 33554432 | tf_op jit(solution)/shard_map/outp/pallas_call | solution.py:526
  694.5 1.7 collective-permute-start.32
  696.6 1.7 collective-permute-start.26
  698.3 90.6 %mlp.6 = (bf16[256,4096]{1,0:T(8,128)(2,1)}, bf16[256,4096]{1,0:T(8,128)(2,1)}) custom-call(bf16[256,4096]{1,0:T(8,128)(2,1)} %get-tuple-element.113.refs_0_, bf16[256,4096]{1,0:T(8,128)(2,1)} %collective-permute-done.27.refs_1_, bf16[4096,3072]{1,0:T(8,128)(2,1)} %refs_2_.9, bf16[4096,3072]{1,0:T(8,128)(2,1)} %refs_3_.9, bf16[3072,4096]{1,0:T(8,128)(2,1)} %refs_4_.9, ...), custom_call_target="tpu_custom_call" | custom-call | flops 77309411328 | bytes 75497472 | tf_op jit(solution)/shard_map/mlp/pallas_call | solution.py:688
  789.2 44.1 %collective-permute-done.26.refs_1_ = bf16[256,4096]{1,0:T(8,128)(2,1)} collective-permute-done((bf16[256,4096]{1,0:T(8,128)(2,1)}, bf16[256,4096]{1,0:T(8,128)(2,1)}, u32[]{:S(2)}, u32[]{:S(2)}) %collective-permute-start.26) | collective-permute-done | bytes 2097184 | tf_op jit(solution)/shard_map/ppermute | solution.py:828
  833.2 4.9 zsum.5.refs_5_.refs_0_
  838.2 90.4 %mlp.7 = (bf16[256,4096]{1,0:T(8,128)(2,1)}, bf16[256,4096]{1,0:T(8,128)(2,1)}) custom-call(bf16[256,4096]{1,0:T(8,128)(2,1)} %get-tuple-element.122.refs_0_, bf16[256,4096]{1,0:T(8,128)(2,1)} %collective-permute-done.32.refs_1_, bf16[4096,3072]{1,0:T(8,128)(2,1)} %refs_2_.9, bf16[4096,3072]{1,0:T(8,128)(2,1)} %refs_3_.9, bf16[3072,4096]{1,0:T(8,128)(2,1)} %refs_4_.9, ...), custom_call_target="tpu_custom_call" | custom-call | flops 77309411328 | bytes 75497472 | tf_op jit(solution)/shard_map/mlp/pallas_call | solution.py:688
  928.6 1.7 collective-permute-start.33
  930.4 4.9 zsum.6.refs_5_.refs_0_
  935.3 49.7 %mlp.8 = (bf16[128,4096]{1,0:T(8,128)(2,1)}, bf16[128,4096]{1,0:T(8,128)(2,1)}) custom-call(bf16[256,4096]{1,0:T(8,128)(2,1)} %get-tuple-element.125.refs_0_, bf16[256,4096]{1,0:T(8,128)(2,1)} %collective-permute-done.34.refs_1_, bf16[4096,3072]{1,0:T(8,128)(2,1)} %refs_2_.9, bf16[4096,3072]{1,0:T(8,128)(2,1)} %refs_3_.9, bf16[3072,4096]{1,0:T(8,128)(2,1)} %refs_4_.9, ...), custom_call_target="tpu_custom_call" | custom-call | flops 38654705664 | bytes 75497472 | tf_op jit(solution)/shard_map/mlp/pallas_call | solution.py:688
  985.3 4.9 zsum.7.refs_5_.refs_0_
  990.3 61.8 %mlp.9.refs_4_.refs_1_ = bf16[128,4096]{1,0:T(8,128)(2,1)} custom-call(bf16[256,4096]{1,0:T(8,128)(2,1)} %get-tuple-element.125.refs_0_, bf16[256,4096]{1,0:T(8,128)(2,1)} %collective-permute-done.34.refs_1_, bf16[4096,3072]{1,0:T(8,128)(2,1)} %refs_2_.9, bf16[4096,3072]{1,0:T(8,128)(2,1)} %refs_3_.9, bf16[3072,4096]{1,0:T(8,128)(2,1)} %refs_4_.9, ...), custom_call_target="tpu_custom_call" | custom-call | flops 38654705664 | bytes 75497472 | tf_op jit(solution)/shard_map/mlp/pallas_call | solution.py:688
  1052.1 2.9 zsum.8.refs_0_
  1055.0 2.4 zsum.9
  (69 shorter events, 23.9 us)
Async XLA Ops:
  4.7 68.3 %collective-permute-start.5 = (bf16[256,4096]{1,0:T(8,128)(2,1)}, bf16[256,4096]{1,0:T(8,128)(2,1)}, u32[]{:S(2)}, u32[]{:S(2)}) collective-permute-start(bf16[256,4096]{1,0:T(8,128)(2,1)} %norm.2.refs_2_.refs_0_), channel_id=1, source_target_pairs={{0,2},{1,3},{2,0},{3,1},{4,6},{5,7},{6,4},{7,5}} | collective-permute-start | bytes 6291464 | tf_op jit(solution)/shard_map/ppermute | solution.py:828
  8.0 27.4 %collective-permute-start = (bf16[256,4096]{1,0:T(8,128)(2,1)}, bf16[256,4096]{1,0:T(8,128)(2,1)}, u32[]{:S(2)}, u32[]{:S(2)}) collective-permute-start(bf16[256,4096]{1,0:T(8,128)(2,1)} %norm.2.refs_2_.refs_0_), channel_id=1, source_target_pairs={{0,1},{1,0},{2,3},{3,2},{4,5},{5,4},{6,7},{7,6}} | collective-permute-start | bytes 6291464 | tf_op jit(solution)/shard_map/ppermute | solution.py:828
  16.7 18.7 %collective-permute-start.1 = (bf16[256,4096]{1,0:T(8,128)(2,1)}, bf16[256,4096]{1,0:T(8,128)(2,1)}, u32[]{:S(2)}, u32[]{:S(2)}) collective-permute-start(bf16[256,4096]{1,0:T(8,128)(2,1)} %get-tuple-element.67.refs_1_), channel_id=1, source_target_pairs={{0,1},{1,0},{2,3},{3,2},{4,5},{5,4},{6,7},{7,6}} | collective-permute-start | bytes 6291464 | tf_op jit(solution)/shard_map/ppermute | solution.py:828
  17.2 18.2 %collective-permute-start.2 = (bf16[256,4096]{1,0:T(8,128)(2,1)}, bf16[256,4096]{1,0:T(8,128)(2,1)}, u32[]{:S(2)}, u32[]{:S(2)}) collective-permute-start(bf16[256,4096]{1,0:T(8,128)(2,1)} %get-tuple-element.68.refs_2_), channel_id=1, source_target_pairs={{0,1},{1,0},{2,3},{3,2},{4,5},{5,4},{6,7},{7,6}} | collective-permute-start | bytes 6291464 | tf_op jit(solution)/shard_map/ppermute | solution.py:828
  17.2 18.2 %collective-permute-start.3 = (bf16[256,4096]{1,0:T(8,128)(2,1)}, bf16[256,4096]{1,0:T(8,128)(2,1)}, u32[]{:S(2)}, u32[]{:S(2)}) collective-permute-start(bf16[256,4096]{1,0:T(8,128)(2,1)} %get-tuple-element.69.refs_3_), channel_id=1, source_target_pairs={{0,1},{1,0},{2,3},{3,2},{4,5},{5,4},{6,7},{7,6}} | collective-permute-start | bytes 6291464 | tf_op jit(solution)/shard_map/ppermute | solution.py:828
  17.7 10.9 %copy-start.2 = (f32[64]{0:T(128)}, f32[64]{0:T(128)S(1)}, u32[]{:S(2)}) copy-start(f32[64]{0:T(128)S(1)} %multiply_power_fusion) | copy-start | bytes 772
  19.1 12.3 %copy-start = (bf16[4096,2,128]{2,1,0:T(2,128)(2,1)S(1)}, bf16[4096,2,128]{2,1,0:T(2,128)(2,1)}, u32[]{:S(2)}) copy-start(bf16[4096,2,128]{2,1,0:T(2,128)(2,1)} %param.15) | copy-start | bytes 6291460
  31.4 2.0 copy-start.1
  73.1 4.5 collective-permute-start.6
  73.1 48.3 %collective-permute-start.4 = (bf16[256,4096]{1,0:T(8,128)(2,1)}, bf16[256,4096]{1,0:T(8,128)(2,1)}, u32[]{:S(2)}, u32[]{:S(2)}) collective-permute-start(bf16[256,4096]{1,0:T(8,128)(2,1)} %get-tuple-element.67.refs_1_), channel_id=1, source_target_pairs={{0,2},{1,3},{2,0},{3,1},{4,6},{5,7},{6,4},{7,5}} | collective-permute-start | bytes 6291464 | tf_op jit(solution)/shard_map/ppermute | solution.py:828
  121.4 4.5 collective-permute-start.7
  121.5 68.1 %collective-permute-start.8 = (bf16[256,4096]{1,0:T(8,128)(2,1)}, bf16[256,4096]{1,0:T(8,128)(2,1)}, u32[]{:S(2)}, u32[]{:S(2)}) collective-permute-start(bf16[256,4096]{1,0:T(8,128)(2,1)} %get-tuple-element.68.refs_2_), channel_id=1, source_target_pairs={{0,2},{1,3},{2,0},{3,1},{4,6},{5,7},{6,4},{7,5}} | collective-permute-start | bytes 6291464 | tf_op jit(solution)/shard_map/ppermute | solution.py:828
  189.6 5.1 collective-permute-start.9
  190.6 47.9 %collective-permute-start.10 = (bf16[256,4096]{1,0:T(8,128)(2,1)}, bf16[256,4096]{1,0:T(8,128)(2,1)}, u32[]{:S(2)}, u32[]{:S(2)}) collective-permute-start(bf16[256,4096]{1,0:T(8,128)(2,1)} %get-tuple-element.69.refs_3_), channel_id=1, source_target_pairs={{0,2},{1,3},{2,0},{3,1},{4,6},{5,7},{6,4},{7,5}} | collective-permute-start | bytes 6291464 | tf_op jit(solution)/shard_map/ppermute | solution.py:828
  238.5 5.4 collective-permute-start.11
  238.5 48.8 %collective-permute-start.12 = (bf16[8,2,256,256]{3,2,1,0:T(8,128)(2,1)}, bf16[8,2,256,256]{3,2,1,0:T(8,128)(2,1)}, u32[]{:S(2)}, u32[]{:S(2)}) collective-permute-start(bf16[8,2,256,256]{3,2,1,0:T(8,128)(2,1)} %get-tuple-element.75.refs_5_.refs_3_), channel_id=1, source_target_pairs={{0,4},{4,0},{1,5},{5,1},{2,6},{6,2},{3,7},{7,3}} | collective-permute-start | bytes 6291464 | tf_op jit(solution)/shard_map/ppermute | solution.py:828
  241.3 57.2 %collective-permute-start.13 = (bf16[2,2,256,256]{3,2,1,0:T(8,128)(2,1)}, bf16[2,2,256,256]{3,2,1,0:T(8,128)(2,1)}, u32[]{:S(2)}, u32[]{:S(2)}) collective-permute-start(bf16[2,2,256,256]{3,2,1,0:T(8,128)(2,1)} %get-tuple-element.78.refs_5_.refs_4_), channel_id=1, source_target_pairs={{0,4},{4,0},{1,5},{5,1},{2,6},{6,2},{3,7},{7,3}} | collective-permute-start | bytes 1572872 | tf_op jit(solution)/shard_map/ppermute | solution.py:828
  241.8 68.0 %collective-permute-start.14 = (bf16[2,2,256,256]{3,2,1,0:T(8,128)(2,1)}, bf16[2,2,256,256]{3,2,1,0:T(8,128)(2,1)}, u32[]{:S(2)}, u32[]{:S(2)}) collective-permute-start(bf16[2,2,256,256]{3,2,1,0:T(8,128)(2,1)} %get-tuple-element.81.refs_5_), channel_id=1, source_target_pairs={{0,4},{4,0},{1,5},{5,1},{2,6},{6,2},{3,7},{7,3}} | collective-permute-start | bytes 1572872 | tf_op jit(solution)/shard_map/ppermute | solution.py:828
  243.4 77.6 %collective-permute-start.15 = (bf16[2,2,256,256]{3,2,1,0:T(8,128)(2,1)}, bf16[2,2,256,256]{3,2,1,0:T(8,128)(2,1)}, u32[]{:S(2)}, u32[]{:S(2)}) collective-permute-start(bf16[2,2,256,256]{3,2,1,0:T(8,128)(2,1)} %get-tuple-element.85.refs_5_.refs_6_), channel_id=1, source_target_pairs={{0,4},{4,0},{1,5},{5,1},{2,6},{6,2},{3,7},{7,3}} | collective-permute-start | bytes 1572872 | tf_op jit(solution)/shard_map/ppermute | solution.py:828
  251.7 80.1 %collective-permute-start.16 = (bf16[2,2,256,256]{3,2,1,0:T(8,128)(2,1)}, bf16[2,2,256,256]{3,2,1,0:T(8,128)(2,1)}, u32[]{:S(2)}, u32[]{:S(2)}) collective-permute-start(bf16[2,2,256,256]{3,2,1,0:T(8,128)(2,1)} %qkv.10.refs_5_.refs_7_), channel_id=1, source_target_pairs={{0,4},{4,0},{1,5},{5,1},{2,6},{6,2},{3,7},{7,3}} | collective-permute-start | bytes 1572872 | tf_op jit(solution)/shard_map/ppermute | solution.py:828
  287.3 212.5 %collective-permute-start.20 = (bf16[1024,4096]{1,0:T(8,128)(2,1)}, bf16[1024,4096]{1,0:T(8,128)(2,1)}, u32[]{:S(2)}, u32[]{:S(2)}) collective-permute-start(bf16[1024,4096]{1,0:T(8,128)(2,1)} %bitcast.22), channel_id=1, source_target_pairs={{0,1},{1,0},{2,3},{3,2},{4,5},{5,4},{6,7},{7,6}} | collective-permute-start | bytes 25165832 | tf_op jit(solution)/shard_map/ppermute | solution.py:828
  298.5 106.3 %collective-permute-start.21 = (bf16[256,4096]{1,0:T(8,128)(2,1)}, bf16[256,4096]{1,0:T(8,128)(2,1)}, u32[]{:S(2)}, u32[]{:S(2)}) collective-permute-start(bf16[256,4096]{1,0:T(8,128)(2,1)} %get-tuple-element.97), channel_id=1, source_target_pairs={{0,2},{1,3},{2,0},{3,1},{4,6},{5,7},{6,4},{7,5}} | collective-permute-start | bytes 6291464 | tf_op jit(solution)/shard_map/ppermute | solution.py:828
  309.8 95.1 %collective-permute-start.22 = (bf16[256,4096]{1,0:T(8,128)(2,1)}, bf16[256,4096]{1,0:T(8,128)(2,1)}, u32[]{:S(2)}, u32[]{:S(2)}) collective-permute-start(bf16[256,4096]{1,0:T(8,128)(2,1)} %get-tuple-element.99), channel_id=1, source_target_pairs={{0,2},{1,3},{2,0},{3,1},{4,6},{5,7},{6,4},{7,5}} | collective-permute-start | bytes 6291464 | tf_op jit(solution)/shard_map/ppermute | solution.py:828
  404.8 3.0 collective-permute-start.17
  404.9 47.7 %collective-permute-start.18 = (bf16[2,256,1024]{2,1,0:T(8,128)(2,1)}, bf16[2,256,1024]{2,1,0:T(8,128)(2,1)}, u32[]{:S(2)}, u32[]{:S(2)}) collective-permute-start(bf16[2,256,1024]{2,1,0:T(8,128)(2,1)} %get-tuple-element.94), channel_id=1, source_target_pairs={{0,2},{1,3},{2,0},{3,1},{4,6},{5,7},{6,4},{7,5}} | collective-permute-start | bytes 3145736 | tf_op jit(solution)/shard_map/ppermute | solution.py:828
  406.5 46.2 %collective-permute-start.19 = (bf16[2,256,1024]{2,1,0:T(8,128)(2,1)}, bf16[2,256,1024]{2,1,0:T(8,128)(2,1)}, u32[]{:S(2)}, u32[]{:S(2)}) collective-permute-start(bf16[2,256,1024]{2,1,0:T(8,128)(2,1)} %get-tuple-element.95), channel_id=1, source_target_pairs={{0,3},{1,2},{2,1},{3,0},{4,7},{5,6},{6,5},{7,4}} | collective-permute-start | bytes 3145736 | tf_op jit(solution)/shard_map/ppermute | solution.py:828
  406.7 48.8 %collective-permute-start.23 = (bf16[256,4096]{1,0:T(8,128)(2,1)}, bf16[256,4096]{1,0:T(8,128)(2,1)}, u32[]{:S(2)}, u32[]{:S(2)}) collective-permute-start(bf16[256,4096]{1,0:T(8,128)(2,1)} %collective-permute-done.21.refs_6_), channel_id=1, source_target_pairs={{0,4},{4,0},{1,5},{5,1},{2,6},{6,2},{3,7},{7,3}} | collective-permute-start | bytes 6291464 | tf_op jit(solution)/shard_map/ppermute | solution.py:828
  407.8 92.0 %collective-permute-start.24 = (bf16[256,4096]{1,0:T(8,128)(2,1)}, bf16[256,4096]{1,0:T(8,128)(2,1)}, u32[]{:S(2)}, u32[]{:S(2)}) collective-permute-start(bf16[256,4096]{1,0:T(8,128)(2,1)} %collective-permute-done.22.refs_7_), channel_id=1, source_target_pairs={{0,4},{4,0},{1,5},{5,1},{2,6},{6,2},{3,7},{7,3}} | collective-permute-start | bytes 6291464 | tf_op jit(solution)/shard_map/ppermute | solution.py:828
  528.0 47.7 %collective-permute-start.25 = (bf16[256,4096]{1,0:T(8,128)(2,1)}, bf16[256,4096]{1,0:T(8,128)(2,1)}, u32[]{:S(2)}, u32[]{:S(2)}) collective-permute-start(bf16[256,4096]{1,0:T(8,128)(2,1)} %get-tuple-element.104.refs_0_), channel_id=1, source_target_pairs={{0,2},{1,3},{2,0},{3,1},{4,6},{5,7},{6,4},{7,5}} | collective-permute-start | bytes 6291464 | tf_op jit(solution)/shard_map/ppermute | solution.py:828
  573.6 92.6 %collective-permute-start.28 = (bf16[2,256,1024]{2,1,0:T(8,128)(2,1)}, bf16[2,256,1024]{2,1,0:T(8,128)(2,1)}, u32[]{:S(2)}, u32[]{:S(2)}) collective-permute-start(bf16[2,256,1024]{2,1,0:T(8,128)(2,1)} %get-tuple-element.115), channel_id=1, source_target_pairs={{0,1},{1,0},{2,3},{3,2},{4,5},{5,4},{6,7},{7,6}} | collective-permute-start | bytes 3145736 | tf_op jit(solution)/shard_map/ppermute | solution.py:828
  573.6 92.6 %collective-permute-start.29 = (bf16[2,256,1024]{2,1,0:T(8,128)(2,1)}, bf16[2,256,1024]{2,1,0:T(8,128)(2,1)}, u32[]{:S(2)}, u32[]{:S(2)}) collective-permute-start(bf16[2,256,1024]{2,1,0:T(8,128)(2,1)} %get-tuple-element.116), channel_id=1, source_target_pairs={{0,2},{1,3},{2,0},{3,1},{4,6},{5,7},{6,4},{7,5}} | collective-permute-start | bytes 3145736 | tf_op jit(solution)/shard_map/ppermute | solution.py:828
  573.6 92.6 %collective-permute-start.30 = (bf16[2,256,1024]{2,1,0:T(8,128)(2,1)}, bf16[2,256,1024]{2,1,0:T(8,128)(2,1)}, u32[]{:S(2)}, u32[]{:S(2)}) collective-permute-start(bf16[2,256,1024]{2,1,0:T(8,128)(2,1)} %get-tuple-element.117), channel_id=1, source_target_pairs={{0,3},{1,2},{2,1},{3,0},{4,7},{5,6},{6,5},{7,4}} | collective-permute-start | bytes 3145736 | tf_op jit(solution)/shard_map/ppermute | solution.py:828
  575.5 122.8 %collective-permute-start.27 = (bf16[256,4096]{1,0:T(8,128)(2,1)}, bf16[256,4096]{1,0:T(8,128)(2,1)}, u32[]{:S(2)}, u32[]{:S(2)}) collective-permute-start(bf16[256,4096]{1,0:T(8,128)(2,1)} %get-tuple-element.113.refs_0_), channel_id=1, source_target_pairs={{0,2},{1,3},{2,0},{3,1},{4,6},{5,7},{6,4},{7,5}} | collective-permute-start | bytes 6291464 | tf_op jit(solution)/shard_map/ppermute | solution.py:828
  694.5 143.7 %collective-permute-start.32 = (bf16[256,4096]{1,0:T(8,128)(2,1)}, bf16[256,4096]{1,0:T(8,128)(2,1)}, u32[]{:S(2)}, u32[]{:S(2)}) collective-permute-start(bf16[256,4096]{1,0:T(8,128)(2,1)} %get-tuple-element.122.refs_0_), channel_id=1, source_target_pairs={{0,2},{1,3},{2,0},{3,1},{4,6},{5,7},{6,4},{7,5}} | collective-permute-start | bytes 6291464 | tf_op jit(solution)/shard_map/ppermute | solution.py:828
  696.3 239.0 %collective-permute-start.34 = (bf16[256,4096]{1,0:T(8,128)(2,1)}, bf16[256,4096]{1,0:T(8,128)(2,1)}, u32[]{:S(2)}, u32[]{:S(2)}) collective-permute-start(bf16[256,4096]{1,0:T(8,128)(2,1)} %get-tuple-element.125.refs_0_), channel_id=1, source_target_pairs={{0,2},{1,3},{2,0},{3,1},{4,6},{5,7},{6,4},{7,5}} | collective-permute-start | bytes 6291464 | tf_op jit(solution)/shard_map/ppermute | solution.py:828
  696.6 136.7 %collective-permute-start.26 = (bf16[256,4096]{1,0:T(8,128)(2,1)}, bf16[256,4096]{1,0:T(8,128)(2,1)}, u32[]{:S(2)}, u32[]{:S(2)}) collective-permute-start(bf16[256,4096]{1,0:T(8,128)(2,1)} %get-tuple-element.112), channel_id=1, source_target_pairs={{0,2},{1,3},{2,0},{3,1},{4,6},{5,7},{6,4},{7,5}} | collective-permute-start | bytes 6291464 | tf_op jit(solution)/shard_map/ppermute | solution.py:828
  788.9 141.5 %collective-permute-start.31 = (bf16[256,4096]{1,0:T(8,128)(2,1)}, bf16[256,4096]{1,0:T(8,128)(2,1)}, u32[]{:S(2)}, u32[]{:S(2)}) collective-permute-start(bf16[256,4096]{1,0:T(8,128)(2,1)} %get-tuple-element.120), channel_id=1, source_target_pairs={{0,2},{1,3},{2,0},{3,1},{4,6},{5,7},{6,4},{7,5}} | collective-permute-start | bytes 6291464 | tf_op jit(solution)/shard_map/ppermute | solution.py:828
  928.6 56.7 %collective-permute-start.33 = (bf16[256,4096]{1,0:T(8,128)(2,1)}, bf16[256,4096]{1,0:T(8,128)(2,1)}, u32[]{:S(2)}, u32[]{:S(2)}) collective-permute-start(bf16[256,4096]{1,0:T(8,128)(2,1)} %get-tuple-element.124), channel_id=1, source_target_pairs={{0,2},{1,3},{2,0},{3,1},{4,6},{5,7},{6,4},{7,5}} | collective-permute-start | bytes 6291464 | tf_op jit(solution)/shard_map/ppermute | solution.py:828
  985.0 67.1 %collective-permute-start.35 = (bf16[128,4096]{1,0:T(8,128)(2,1)}, bf16[128,4096]{1,0:T(8,128)(2,1)}, u32[]{:S(2)}, u32[]{:S(2)}) collective-permute-start(bf16[128,4096]{1,0:T(8,128)(2,1)} %get-tuple-element.127), channel_id=1, source_target_pairs={{0,2},{1,3},{2,0},{3,1},{4,6},{5,7},{6,4},{7,5}} | collective-permute-start | bytes 3145736 | tf_op jit(solution)/shard_map/ppermute | solution.py:828

commit v17 on v16

--- a/solution.py
+++ b/solution.py
@@ -431,51 +431,45 @@
     o_scr, w_scr, x_scr, acc_scr, o_sem, w_sem, x_sem, out_sem, sent_sem = refs[n_o + n_w + 2 + n_out:]
     width = o_refs[0].shape[-1]
     half = width // 2
-    n_slots = w_scr.shape[0] - n_shared
     n_local = len(blocks)
+    landing = w_scr.shape[0] - n_shared
+    n_slots = landing - n_shared
     mate = other_core()
     barrier = pltpu.get_barrier_semaphore()
     pl.semaphore_signal(barrier, inc=1, device_id=mate, device_id_type=pl.DeviceIdType.MESH)
 
+    def place(i):
+        return i if i < n_shared else n_shared + (i - n_shared) % n_slots
+
     def fetch(k):
         for i, pieces in enumerate(blocks):
             @pl.when(k == i)
             def _():
                 to = 0
                 for a, r0, n in pieces:
-                    pltpu.make_async_copy(w_refs[a].at[pl.ds(r0, n), :], w_scr.at[i % n_slots, pl.ds(to, n), :],
-                                          w_sem.at[i % n_slots]).start()
+                    pltpu.make_async_copy(w_refs[a].at[pl.ds(r0, n), :], w_scr.at[place(i), pl.ds(to, n), :],
+                                          w_sem.at[place(i)]).start()
                     to += n
 
     mine = lax.axis_index('cp')
     loads = [[] for _ in range(n_local + n_shared)]
     for i in range(n_run):
         rows = pl.ds(i * RUN, RUN)
-        for k in range(4):
+        for k, at_block in enumerate((n_shared, 2 * n_shared, 0, n_local)):
             src = o_refs[k].at[i]
-            if k < 2:
-                loads[2 * k].append((src, o_scr.at[rows, pl.ds(k * width, width)]))
-            else:
-                for p, part in enumerate((mine, 1 - mine)):
-                    loads[2 * k + p].append((src.at[:, pl.ds(pl.multiple_of(part * half, half), half)],
-                                             o_scr.at[rows, pl.ds(k * width + p * half, half)]))
+            for p, part in enumerate((mine, 1 - mine) if at_block in (0, n_local) else PAIR):
+                loads[at_block + p].append((src.at[:, pl.ds(pl.multiple_of(part * half, half), half)],
+                                            o_scr.at[rows, pl.ds((at_block + p) * half, half)]))
     copies = [[pltpu.make_async_copy(src, dst, o_sem.at[k, i]) for i, (src, dst) in enumerate(ls)] for k, ls in enumerate(loads)]
     x_copy = pltpu.make_async_copy(x_ref.at[pl.ds(at * n_run * RUN, n_run * RUN), :], x_scr, x_sem)
     for cp in copies[0]:
         cp.start()
-    for i in range(n_slots - 1):
+    for i in range(n_slots):
         fetch(jnp.int32(i))
-    shared = []
     pl.semaphore_wait(barrier, 1)
-    for b in range(n_shared):
-        to = 0
-        for a, r0, n in blocks[b - n_shared]:
-            shared.append(pltpu.make_async_remote_copy(
-                src_ref=w_refs[a].at[pl.ds(r0, n), :], dst_ref=w_scr.at[n_slots + b, pl.ds(to, n), :],
-                send_sem=sent_sem.at[len(shared)], recv_sem=w_sem.at[n_slots + b], device_id=mate,
-                device_id_type=pl.DeviceIdType.MESH))
-            shared[-1].start()
-            to += n
+    shared = [pltpu.make_async_remote_copy(
+        src_ref=w_scr.at[b], dst_ref=w_scr.at[landing + b], send_sem=sent_sem.at[b], recv_sem=w_sem.at[landing + b],
+        device_id=mate, device_id_type=pl.DeviceIdType.MESH) for b in range(n_shared)]
     for ls in copies[1:]:
         for cp in ls:
             cp.start()
@@ -483,15 +477,22 @@
     acc_scr[:] = jnp.zeros_like(acc_scr)
 
     def one(k, carry):
-        fetch(k + n_slots - 1)
+        @pl.when(k > 0)
+        def _():
+            fetch(k + n_slots - 1)
+
         for i, ls in enumerate(copies):
-            if ls:
-                @pl.when(k == i)
-                def _():
-                    for cp in ls:
-                        cp.wait()
-        slot = jnp.where(k < n_local, lax.rem(k, n_slots), k - n_local + n_slots)
+            @pl.when(k == i)
+            def _():
+                for cp in ls:
+                    cp.wait()
+        turn = jnp.where(k < n_shared, k, n_shared + lax.rem(k - n_shared + n_slots, n_slots))
+        slot = jnp.where(k < n_local, turn, k - n_local + landing)
         pltpu.make_async_copy(w_scr.at[slot], w_scr.at[slot], w_sem.at[slot]).wait()
+        for b, cp in enumerate(shared):
+            @pl.when(k == b)
+            def _():
+                cp.start()
         acc_scr[:] += jnp.dot(o_scr[:, pl.ds(pl.multiple_of(k * half, half), half)], w_scr[slot], preferred_element_type=F32)
         return carry
 
@@ -523,6 +524,7 @@
     dim = x_rows.shape[1]
     n_run, _, width = os[0].shape
     rows = n_run * RUN
+    n_w = 3 + 2 * n_shared
     return pl.pallas_call(
         ordered(functools.partial(out_kernel, blocks=blocks, n_w=len(ws), n_run=n_run, at=at, n_shared=n_shared),
                 len(os) + len(ws) + 2, after),
@@ -530,10 +532,10 @@
         in_specs=[ANY] * (len(os) + len(ws) + 1) + [pl.BlockSpec((1, dim), lambda i: (0, 0))] + [ANY] * len(after),
         out_specs=[ANY] * (2 * n_run),
         out_shape=[jax.ShapeDtypeStruct((RUN, dim), BF)] * (2 * n_run),
-        scratch_shapes=[pltpu.VMEM((rows, 4 * width), BF), pltpu.VMEM((3 + n_shared, width // 2, dim), BF), pltpu.VMEM((rows, dim), BF),
+        scratch_shapes=[pltpu.VMEM((rows, 4 * width), BF), pltpu.VMEM((n_w, width // 2, dim), BF), pltpu.VMEM((rows, dim), BF),
                         pltpu.VMEM((rows, dim), F32), pltpu.SemaphoreType.DMA((len(blocks) + n_shared, 2 * n_run)),
-                        pltpu.SemaphoreType.DMA((3 + n_shared,)), pltpu.SemaphoreType.DMA, pltpu.SemaphoreType.DMA((2 * n_run,)),
-                        pltpu.SemaphoreType.DMA((len(ws),))],
+                        pltpu.SemaphoreType.DMA((n_w,)), pltpu.SemaphoreType.DMA, pltpu.SemaphoreType.DMA((2 * n_run,)),
+                        pltpu.SemaphoreType.DMA((n_shared,))],
         name="outp",
         compiler_params=pltpu.CompilerParams(vmem_limit_bytes=VMEM, collective_id=call, has_side_effects=True),
         cost_estimate=cost(8 * rows * width * dim, 8 * width * dim),
@@ -890,8 +892,8 @@
 
         def project(i):
             ws = [wo, wo_c, *wo_a, *wo_b]
-            blocks = [[(a, r, half)] for a in PAIR for r in (0, half)]
-            blocks += [[(2 + b * n_piece + p, 0, rows) for p in range(n_piece)] for b in PAIR]
+            blocks = [[(2 + b * n_piece + p, 0, rows) for p in range(n_piece)] for b in PAIR]
+            blocks += [[(a, r, half)] for a in PAIR for r in (0, half)]
             got = out_proj(os[i], ws, blocks, 2, x_rows, gm, i, n_run + 1 + i, after=(prev,))
             for y, b in zip(got[::2], got[1::2]):
                 outs.append((y, b, send(over_x, b)))

time: 1070 us -> 1070 us (level)
  no operation moved by 1% of the time
where the time goes in v17:
time: 1070 us; the launch traced here: 1060 us
  Pallas kernels  782 us (73%)
  waiting for transfers between devices  223 us (21%)
  starting transfers between devices  28.2 us (3%)
  local copies, waits for them, and re-layouts  18.8 us (2%)
    pallas_call x5, Pallas kernels, mlp(): pl.pallas_call(ordered(functools.partial(mlp_kernel, n_in=len(bs), first=...  383 us
    ppermute x36, waiting for transfers between devices, send(): return lax.ppermute(v, *axis_pairs)  223 us
    pallas_call x5, Pallas kernels, flash(): pl.pallas_call(ordered(functools.partial(flash_kernel, q_src=q_src, kv_sr...  211 us
    pallas_call x6, Pallas kernels, qkv(): pl.pallas_call(ordered(functools.partial(qkv_kernel, n_in=n_in, n_q=n_q,...  97.6 us
    pallas_call x2, Pallas kernels, out_proj(): pl.pallas_call(ordered(functools.partial(out_kernel, blocks=blocks, n_w=l...  58.6 us
    ppermute x36, starting transfers between devices, send(): return lax.ppermute(v, *axis_pairs)  28.2 us
  transfers between devices with their start and end apart: 36, of which 15 were waited for; matrix products, arithmetic and copies ran while one was open for 2% of the time, Pallas kernels for 70%

profile of v17, /device:TPU:0, one launch (start us, length us, event | category | flops | bytes accessed | tf_op | source)
XLA Modules:
  0.0 1059.8 jit_solution(6003443902480061851)
XLA Ops:
  1.3 3.4 norm.2.refs_2_.refs_0_
  4.7 3.3 collective-permute-start.5
  8.0 8.6 norm.3
  19.1 9.5 bitcast_dynamic-update-slice_fusion
  28.6 2.8 multiply_sine_fusion.1
  31.4 2.0 bitcast_dynamic-update-slice_fusion.2
  33.4 2.0 bitcast_dynamic-update-slice_fusion.1.refs_8_.refs_2_
  35.4 37.6 %qkv.6 = (bf16[8,1024,256]{2,1,0:T(8,128)(2,1)}, bf16[8,2,256,256]{3,2,1,0:T(8,128)(2,1)}) custom-call(bf16[256,4096]{1,0:T(8,128)(2,1)} %norm.2.refs_2_.refs_0_, bf16[256,4096]{1,0:T(8,128)(2,1)} %get-tuple-element.67.refs_1_, bf16[256,4096]{1,0:T(8,128)(2,1)} %get-tuple-element.68.refs_2_, bf16[256,4096]{1,0:T(8,128)(2,1)} %get-tuple-element.69.refs_3_, ...), custom_call_target="tpu_custom_call" | custom-call | flops 25769803776 | bytes 12582912 | tf_op jit(solution)/shard_map/qkv/pallas_call | solution.py:139
  73.8 3.4 multiply_sine_fusion
  77.6 14.0 %qkv.7 = (bf16[2,1024,256]{2,1,0:T(8,128)(2,1)}, bf16[2,2,256,256]{3,2,1,0:T(8,128)(2,1)}) custom-call(bf16[256,4096]{1,0:T(8,128)(2,1)} %collective-permute-done.5.refs_0_, bf16[256,4096]{1,0:T(8,128)(2,1)} %collective-permute-done.6.refs_1_, bf16[4096,1536]{1,0:T(8,128)(2,1)} %bitcast_dynamic-update-slice_fusion.1.refs_8_.refs_2_, ...), custom_call_target="tpu_custom_call" | custom-call | flops 6442450944 | bytes 12582912 | tf_op jit(solution)/shard_map/qkv/pallas_call | solution.py:139
  91.6 29.8 %collective-permute-done.4.refs_0_ = bf16[256,4096]{1,0:T(8,128)(2,1)} collective-permute-done((bf16[256,4096]{1,0:T(8,128)(2,1)}, bf16[256,4096]{1,0:T(8,128)(2,1)}, u32[]{:S(2)}, u32[]{:S(2)}) %collective-permute-start.4) | collective-permute-done | bytes 2097184 | tf_op jit(solution)/shard_map/ppermute | solution.py:830
  123.1 2.9 collective-permute-done.7.refs_1_
  126.0 13.6 %qkv.8 = (bf16[2,1024,256]{2,1,0:T(8,128)(2,1)}, bf16[2,2,256,256]{3,2,1,0:T(8,128)(2,1)}) custom-call(bf16[256,4096]{1,0:T(8,128)(2,1)} %collective-permute-done.4.refs_0_, bf16[256,4096]{1,0:T(8,128)(2,1)} %collective-permute-done.7.refs_1_, bf16[4096,1536]{1,0:T(8,128)(2,1)} %bitcast_dynamic-update-slice_fusion.1.refs_8_.refs_2_, ...), custom_call_target="tpu_custom_call" | custom-call | flops 6442450944 | bytes 12582912 | tf_op jit(solution)/shard_map/qkv/pallas_call | solution.py:139
  139.5 50.0 %flash_part.1 = (f32[10,2,4,144,256]{4,3,2,1,0:T(8,128)}, bf16[256,4096]{1,0:T(8,128)(2,1)}, bf16[256,4096]{1,0:T(8,128)(2,1)}) custom-call(s32[845]{0:T(1024)} %dynamic-slice_reduce_fusion.refs_0_, bf16[8,1024,256]{2,1,0:T(8,128)(2,1)} %get-tuple-element.74.refs_1_, bf16[2,1024,256]{2,1,0:T(8,128)(2,1)} %get-tuple-element.82.refs_2_, ...), custom_call_target="tpu_custom_call" | custom-call | flops 38654705664 | bytes 3145728 | tf_op jit(solution)/shard_map/flash_part/pallas_call | solution.py:398
  191.7 3.0 collective-permute-done.9.refs_1_
  194.7 13.7 %qkv.9 = (bf16[2,1024,256]{2,1,0:T(8,128)(2,1)}, bf16[2,2,256,256]{3,2,1,0:T(8,128)(2,1)}) custom-call(bf16[256,4096]{1,0:T(8,128)(2,1)} %collective-permute-done.8.refs_0_, bf16[256,4096]{1,0:T(8,128)(2,1)} %collective-permute-done.9.refs_1_, bf16[4096,1536]{1,0:T(8,128)(2,1)} %bitcast_dynamic-update-slice_fusion.1.refs_8_.refs_2_, ...), custom_call_target="tpu_custom_call" | custom-call | flops 6442450944 | bytes 12582912 | tf_op jit(solution)/shard_map/qkv/pallas_call | solution.py:139
  208.5 30.0 %collective-permute-done.10.refs_0_ = bf16[256,4096]{1,0:T(8,128)(2,1)} collective-permute-done((bf16[256,4096]{1,0:T(8,128)(2,1)}, bf16[256,4096]{1,0:T(8,128)(2,1)}, u32[]{:S(2)}, u32[]{:S(2)}) %collective-permute-start.10) | collective-permute-done | bytes 2097184 | tf_op jit(solution)/shard_map/ppermute | solution.py:830
  243.8 7.8 qkv.10.refs_5_.refs_7_
  253.2 10.8 %qkv.11.refs_14_.refs_2_ = bf16[2,1024,256]{2,1,0:T(8,128)(2,1)} custom-call(bf16[256,4096]{1,0:T(8,128)(2,1)} %collective-permute-done.10.refs_0_, bf16[256,4096]{1,0:T(8,128)(2,1)} %collective-permute-done.11.refs_1_, bf16[4096,1536]{1,0:T(8,128)(2,1)} %bitcast_dynamic-update-slice_fusion.1.refs_8_.refs_2_, f32[8,64,256]{2,1,0:T(8,128)} %get-tuple-element.132.refs_3_, ...), custom_call_target="tpu_custom_call" | custom-call | flops 6442450944 | bytes 12582912 | tf_op jit(solution)/shard_map/qkv/pallas_call | solution.py:139
  264.0 23.3 %collective-permute-done.12.refs_8_ = bf16[8,2,256,256]{3,2,1,0:T(8,128)(2,1)} collective-permute-done((bf16[8,2,256,256]{3,2,1,0:T(8,128)(2,1)}, bf16[8,2,256,256]{3,2,1,0:T(8,128)(2,1)}, u32[]{:S(2)}, u32[]{:S(2)}) %collective-permute-start.12) | collective-permute-done | bytes 2097184 | tf_op jit(solution)/shard_map/ppermute | solution.py:830
  287.3 11.2 %collective-permute-done.13.refs_9_ = bf16[2,2,256,256]{3,2,1,0:T(8,128)(2,1)} collective-permute-done((bf16[2,2,256,256]{3,2,1,0:T(8,128)(2,1)}, bf16[2,2,256,256]{3,2,1,0:T(8,128)(2,1)}, u32[]{:S(2)}, u32[]{:S(2)}) %collective-permute-start.13) | collective-permute-done | bytes 524320 | tf_op jit(solution)/shard_map/ppermute | solution.py:830
  300.1 9.7 collective-permute-done.14.refs_10_
  311.3 9.7 collective-permute-done.15.refs_11_
  321.0 10.8 %collective-permute-done.16.refs_12_ = bf16[2,2,256,256]{3,2,1,0:T(8,128)(2,1)} collective-permute-done((bf16[2,2,256,256]{3,2,1,0:T(8,128)(2,1)}, bf16[2,2,256,256]{3,2,1,0:T(8,128)(2,1)}, u32[]{:S(2)}, u32[]{:S(2)}) %collective-permute-start.16) | collective-permute-done | bytes 524320 | tf_op jit(solution)/shard_map/ppermute | solution.py:830
  331.8 29.1 %flash.4 = (bf16[2,256,1024]{2,1,0:T(8,128)(2,1)}, bf16[2,256,1024]{2,1,0:T(8,128)(2,1)}, bf16[2,256,1024]{2,1,0:T(8,128)(2,1)}, bf16[2,256,1024]{2,1,0:T(8,128)(2,1)}, f32[8,128]{1,0:T(8,128)}) custom-call(s32[845]{0:T(1024)} %dynamic-slice_reduce_fusion.refs_0_, bf16[8,1024,256]{2,1,0:T(8,128)(2,1)} %get-tuple-element.74.refs_1_, ...), custom_call_target="tpu_custom_call" | custom-call | flops 23622320128 | bytes 8388608 | tf_op jit(solution)/shard_map/flash/pallas_call | solution.py:398
  360.9 43.9 %flash.5 = (bf16[2,256,1024]{2,1,0:T(8,128)(2,1)}, bf16[2,256,1024]{2,1,0:T(8,128)(2,1)}, bf16[2,256,1024]{2,1,0:T(8,128)(2,1)}, bf16[2,256,1024]{2,1,0:T(8,128)(2,1)}, f32[8,128]{1,0:T(8,128)}) custom-call(s32[845]{0:T(1024)} %dynamic-slice_reduce_fusion.refs_0_, ...), custom_call_target="tpu_custom_call", output_to_operand_aliasing={{0}: (14, {}), {1}: (15, {}), {2}: (16, {}), {3}: (17, {})} | custom-call | flops 32212254720 | bytes 8388608 | tf_op jit(solution)/shard_map/flash/pallas_call | solution.py:398
  404.9 1.7 collective-permute-start.18
  408.7 43.8 %flash.6 = (bf16[2,256,1024]{2,1,0:T(8,128)(2,1)}, bf16[2,256,1024]{2,1,0:T(8,128)(2,1)}, bf16[2,256,1024]{2,1,0:T(8,128)(2,1)}, bf16[2,256,1024]{2,1,0:T(8,128)(2,1)}, f32[8,128]{1,0:T(8,128)}) custom-call(s32[845]{0:T(1024)} %dynamic-slice_reduce_fusion.refs_0_, bf16[8,1024,256]{2,1,0:T(8,128)(2,1)} %get-tuple-element.74.refs_1_, ...), custom_call_target="tpu_custom_call" | custom-call | flops 32212254720 | bytes 8388608 | tf_op jit(solution)/shard_map/flash/pallas_call | solution.py:398
  452.7 2.8 collective-permute-done.23.refs_8_
  455.5 44.3 %collective-permute-done.24.refs_9_ = bf16[256,4096]{1,0:T(8,128)(2,1)} collective-permute-done((bf16[256,4096]{1,0:T(8,128)(2,1)}, bf16[256,4096]{1,0:T(8,128)(2,1)}, u32[]{:S(2)}, u32[]{:S(2)}) %collective-permute-start.24) | collective-permute-done | bytes 2097184 | tf_op jit(solution)/shard_map/ppermute | solution.py:830
  499.8 29.3 %outp.2 = (bf16[256,4096]{1,0:T(8,128)(2,1)}, bf16[256,4096]{1,0:T(8,128)(2,1)}, bf16[256,4096]{1,0:T(8,128)(2,1)}, bf16[256,4096]{1,0:T(8,128)(2,1)}) custom-call(bf16[2,256,1024]{2,1,0:T(8,128)(2,1)} %get-tuple-element.92.refs_0_, bf16[2,256,1024]{2,1,0:T(8,128)(2,1)} %collective-permute-done.17.refs_1_, ...), custom_call_target="tpu_custom_call" | custom-call | flops 17179869184 | bytes 33554432 | tf_op jit(solution)/shard_map/outp/pallas_call | solution.py:528
  530.8 43.9 %flash.7 = (bf16[2,256,1024]{2,1,0:T(8,128)(2,1)}, bf16[2,256,1024]{2,1,0:T(8,128)(2,1)}, bf16[2,256,1024]{2,1,0:T(8,128)(2,1)}, bf16[2,256,1024]{2,1,0:T(8,128)(2,1)}, f32[8,128]{1,0:T(8,128)}) custom-call(s32[845]{0:T(1024)} %dynamic-slice_reduce_fusion.refs_0_, ...), custom_call_target="tpu_custom_call", output_to_operand_aliasing={{0}: (14, {}), {1}: (15, {}), {2}: (16, {}), {3}: (17, {})} | custom-call | flops 32212254720 | bytes 8388608 | tf_op jit(solution)/shard_map/flash/pallas_call | solution.py:398
  574.8 1.8 collective-permute-start.30
  576.9 90.4 %mlp.5 = (bf16[256,4096]{1,0:T(8,128)(2,1)}, bf16[256,4096]{1,0:T(8,128)(2,1)}) custom-call(bf16[256,4096]{1,0:T(8,128)(2,1)} %get-tuple-element.104.refs_0_, bf16[256,4096]{1,0:T(8,128)(2,1)} %collective-permute-done.25.refs_1_, bf16[4096,3072]{1,0:T(8,128)(2,1)} %refs_2_.9, bf16[4096,3072]{1,0:T(8,128)(2,1)} %refs_3_.9, bf16[3072,4096]{1,0:T(8,128)(2,1)} %refs_4_.9, ...), custom_call_target="tpu_custom_call" | custom-call | flops 77309411328 | bytes 75497472 | tf_op jit(solution)/shard_map/mlp/pallas_call | solution.py:690
  667.3 29.3 %outp.3 = (bf16[256,4096]{1,0:T(8,128)(2,1)}, bf16[256,4096]{1,0:T(8,128)(2,1)}, bf16[256,4096]{1,0:T(8,128)(2,1)}, bf16[256,4096]{1,0:T(8,128)(2,1)}) custom-call(bf16[2,256,1024]{2,1,0:T(8,128)(2,1)} %get-tuple-element.114.refs_0_, bf16[2,256,1024]{2,1,0:T(8,128)(2,1)} %collective-permute-done.28.refs_1_, ...), custom_call_target="tpu_custom_call" | custom-call | flops 17179869184 | bytes 33554432 | tf_op jit(solution)/shard_map/outp/pallas_call | solution.py:528
  696.7 1.7 collective-permute-start.32
  698.7 1.7 collective-permute-start.26
  700.5 90.6 %mlp.6 = (bf16[256,4096]{1,0:T(8,128)(2,1)}, bf16[256,4096]{1,0:T(8,128)(2,1)}) custom-call(bf16[256,4096]{1,0:T(8,128)(2,1)} %get-tuple-element.113.refs_0_, bf16[256,4096]{1,0:T(8,128)(2,1)} %collective-permute-done.27.refs_1_, bf16[4096,3072]{1,0:T(8,128)(2,1)} %refs_2_.9, bf16[4096,3072]{1,0:T(8,128)(2,1)} %refs_3_.9, bf16[3072,4096]{1,0:T(8,128)(2,1)} %refs_4_.9, ...), custom_call_target="tpu_custom_call" | custom-call | flops 77309411328 | bytes 75497472 | tf_op jit(solution)/shard_map/mlp/pallas_call | solution.py:690
  791.4 44.0 %collective-permute-done.26.refs_1_ = bf16[256,4096]{1,0:T(8,128)(2,1)} collective-permute-done((bf16[256,4096]{1,0:T(8,128)(2,1)}, bf16[256,4096]{1,0:T(8,128)(2,1)}, u32[]{:S(2)}, u32[]{:S(2)}) %collective-permute-start.26) | collective-permute-done | bytes 2097184 | tf_op jit(solution)/shard_map/ppermute | solution.py:830
  835.4 4.9 zsum.5.refs_5_.refs_0_
  840.3 90.4 %mlp.7 = (bf16[256,4096]{1,0:T(8,128)(2,1)}, bf16[256,4096]{1,0:T(8,128)(2,1)}) custom-call(bf16[256,4096]{1,0:T(8,128)(2,1)} %get-tuple-element.122.refs_0_, bf16[256,4096]{1,0:T(8,128)(2,1)} %collective-permute-done.32.refs_1_, bf16[4096,3072]{1,0:T(8,128)(2,1)} %refs_2_.9, bf16[4096,3072]{1,0:T(8,128)(2,1)} %refs_3_.9, bf16[3072,4096]{1,0:T(8,128)(2,1)} %refs_4_.9, ...), custom_call_target="tpu_custom_call" | custom-call | flops 77309411328 | bytes 75497472 | tf_op jit(solution)/shard_map/mlp/pallas_call | solution.py:690
  930.8 1.7 collective-permute-start.33
  932.5 4.9 zsum.6.refs_5_.refs_0_
  937.5 49.7 %mlp.8 = (bf16[128,4096]{1,0:T(8,128)(2,1)}, bf16[128,4096]{1,0:T(8,128)(2,1)}) custom-call(bf16[256,4096]{1,0:T(8,128)(2,1)} %get-tuple-element.125.refs_0_, bf16[256,4096]{1,0:T(8,128)(2,1)} %collective-permute-done.34.refs_1_, bf16[4096,3072]{1,0:T(8,128)(2,1)} %refs_2_.9, bf16[4096,3072]{1,0:T(8,128)(2,1)} %refs_3_.9, bf16[3072,4096]{1,0:T(8,128)(2,1)} %refs_4_.9, ...), custom_call_target="tpu_custom_call" | custom-call | flops 38654705664 | bytes 75497472 | tf_op jit(solution)/shard_map/mlp/pallas_call | solution.py:690
  987.5 4.9 zsum.7.refs_5_.refs_0_
  992.4 61.8 %mlp.9.refs_4_.refs_1_ = bf16[128,4096]{1,0:T(8,128)(2,1)} custom-call(bf16[256,4096]{1,0:T(8,128)(2,1)} %get-tuple-element.125.refs_0_, bf16[256,4096]{1,0:T(8,128)(2,1)} %collective-permute-done.34.refs_1_, bf16[4096,3072]{1,0:T(8,128)(2,1)} %refs_2_.9, bf16[4096,3072]{1,0:T(8,128)(2,1)} %refs_3_.9, bf16[3072,4096]{1,0:T(8,128)(2,1)} %refs_4_.9, ...), custom_call_target="tpu_custom_call" | custom-call | flops 38654705664 | bytes 75497472 | tf_op jit(solution)/shard_map/mlp/pallas_call | solution.py:690
  1054.3 2.9 zsum.8.refs_0_
  1057.2 2.4 zsum.9
  (69 shorter events, 23.9 us)
Async XLA Ops:
  4.7 68.3 %collective-permute-start.5 = (bf16[256,4096]{1,0:T(8,128)(2,1)}, bf16[256,4096]{1,0:T(8,128)(2,1)}, u32[]{:S(2)}, u32[]{:S(2)}) collective-permute-start(bf16[256,4096]{1,0:T(8,128)(2,1)} %norm.2.refs_2_.refs_0_), channel_id=1, source_target_pairs={{0,2},{1,3},{2,0},{3,1},{4,6},{5,7},{6,4},{7,5}} | collective-permute-start | bytes 6291464 | tf_op jit(solution)/shard_map/ppermute | solution.py:830
  8.0 27.4 %collective-permute-start = (bf16[256,4096]{1,0:T(8,128)(2,1)}, bf16[256,4096]{1,0:T(8,128)(2,1)}, u32[]{:S(2)}, u32[]{:S(2)}) collective-permute-start(bf16[256,4096]{1,0:T(8,128)(2,1)} %norm.2.refs_2_.refs_0_), channel_id=1, source_target_pairs={{0,1},{1,0},{2,3},{3,2},{4,5},{5,4},{6,7},{7,6}} | collective-permute-start | bytes 6291464 | tf_op jit(solution)/shard_map/ppermute | solution.py:830
  16.7 18.7 %collective-permute-start.1 = (bf16[256,4096]{1,0:T(8,128)(2,1)}, bf16[256,4096]{1,0:T(8,128)(2,1)}, u32[]{:S(2)}, u32[]{:S(2)}) collective-permute-start(bf16[256,4096]{1,0:T(8,128)(2,1)} %get-tuple-element.67.refs_1_), channel_id=1, source_target_pairs={{0,1},{1,0},{2,3},{3,2},{4,5},{5,4},{6,7},{7,6}} | collective-permute-start | bytes 6291464 | tf_op jit(solution)/shard_map/ppermute | solution.py:830
  17.2 18.2 %collective-permute-start.2 = (bf16[256,4096]{1,0:T(8,128)(2,1)}, bf16[256,4096]{1,0:T(8,128)(2,1)}, u32[]{:S(2)}, u32[]{:S(2)}) collective-permute-start(bf16[256,4096]{1,0:T(8,128)(2,1)} %get-tuple-element.68.refs_2_), channel_id=1, source_target_pairs={{0,1},{1,0},{2,3},{3,2},{4,5},{5,4},{6,7},{7,6}} | collective-permute-start | bytes 6291464 | tf_op jit(solution)/shard_map/ppermute | solution.py:830
  17.2 18.2 %collective-permute-start.3 = (bf16[256,4096]{1,0:T(8,128)(2,1)}, bf16[256,4096]{1,0:T(8,128)(2,1)}, u32[]{:S(2)}, u32[]{:S(2)}) collective-permute-start(bf16[256,4096]{1,0:T(8,128)(2,1)} %get-tuple-element.69.refs_3_), channel_id=1, source_target_pairs={{0,1},{1,0},{2,3},{3,2},{4,5},{5,4},{6,7},{7,6}} | collective-permute-start | bytes 6291464 | tf_op jit(solution)/shard_map/ppermute | solution.py:830
  17.7 10.9 %copy-start.2 = (f32[64]{0:T(128)}, f32[64]{0:T(128)S(1)}, u32[]{:S(2)}) copy-start(f32[64]{0:T(128)S(1)} %multiply_power_fusion) | copy-start | bytes 772
  19.1 12.3 %copy-start = (bf16[4096,2,128]{2,1,0:T(2,128)(2,1)S(1)}, bf16[4096,2,128]{2,1,0:T(2,128)(2,1)}, u32[]{:S(2)}) copy-start(bf16[4096,2,128]{2,1,0:T(2,128)(2,1)} %param.15) | copy-start | bytes 6291460
  31.4 2.0 copy-start.1
  73.1 4.5 collective-permute-start.6
  73.1 48.3 %collective-permute-start.4 = (bf16[256,4096]{1,0:T(8,128)(2,1)}, bf16[256,4096]{1,0:T(8,128)(2,1)}, u32[]{:S(2)}, u32[]{:S(2)}) collective-permute-start(bf16[256,4096]{1,0:T(8,128)(2,1)} %get-tuple-element.67.refs_1_), channel_id=1, source_target_pairs={{0,2},{1,3},{2,0},{3,1},{4,6},{5,7},{6,4},{7,5}} | collective-permute-start | bytes 6291464 | tf_op jit(solution)/shard_map/ppermute | solution.py:830
  121.4 4.5 collective-permute-start.7
  121.5 68.1 %collective-permute-start.8 = (bf16[256,4096]{1,0:T(8,128)(2,1)}, bf16[256,4096]{1,0:T(8,128)(2,1)}, u32[]{:S(2)}, u32[]{:S(2)}) collective-permute-start(bf16[256,4096]{1,0:T(8,128)(2,1)} %get-tuple-element.68.refs_2_), channel_id=1, source_target_pairs={{0,2},{1,3},{2,0},{3,1},{4,6},{5,7},{6,4},{7,5}} | collective-permute-start | bytes 6291464 | tf_op jit(solution)/shard_map/ppermute | solution.py:830
  189.6 5.1 collective-permute-start.9
  190.6 47.9 %collective-permute-start.10 = (bf16[256,4096]{1,0:T(8,128)(2,1)}, bf16[256,4096]{1,0:T(8,128)(2,1)}, u32[]{:S(2)}, u32[]{:S(2)}) collective-permute-start(bf16[256,4096]{1,0:T(8,128)(2,1)} %get-tuple-element.69.refs_3_), channel_id=1, source_target_pairs={{0,2},{1,3},{2,0},{3,1},{4,6},{5,7},{6,4},{7,5}} | collective-permute-start | bytes 6291464 | tf_op jit(solution)/shard_map/ppermute | solution.py:830
  238.5 5.4 collective-permute-start.11
  238.5 48.8 %collective-permute-start.12 = (bf16[8,2,256,256]{3,2,1,0:T(8,128)(2,1)}, bf16[8,2,256,256]{3,2,1,0:T(8,128)(2,1)}, u32[]{:S(2)}, u32[]{:S(2)}) collective-permute-start(bf16[8,2,256,256]{3,2,1,0:T(8,128)(2,1)} %get-tuple-element.75.refs_5_.refs_3_), channel_id=1, source_target_pairs={{0,4},{4,0},{1,5},{5,1},{2,6},{6,2},{3,7},{7,3}} | collective-permute-start | bytes 6291464 | tf_op jit(solution)/shard_map/ppermute | solution.py:830
  241.3 57.2 %collective-permute-start.13 = (bf16[2,2,256,256]{3,2,1,0:T(8,128)(2,1)}, bf16[2,2,256,256]{3,2,1,0:T(8,128)(2,1)}, u32[]{:S(2)}, u32[]{:S(2)}) collective-permute-start(bf16[2,2,256,256]{3,2,1,0:T(8,128)(2,1)} %get-tuple-element.78.refs_5_.refs_4_), channel_id=1, source_target_pairs={{0,4},{4,0},{1,5},{5,1},{2,6},{6,2},{3,7},{7,3}} | collective-permute-start | bytes 1572872 | tf_op jit(solution)/shard_map/ppermute | solution.py:830
  241.8 68.0 %collective-permute-start.14 = (bf16[2,2,256,256]{3,2,1,0:T(8,128)(2,1)}, bf16[2,2,256,256]{3,2,1,0:T(8,128)(2,1)}, u32[]{:S(2)}, u32[]{:S(2)}) collective-permute-start(bf16[2,2,256,256]{3,2,1,0:T(8,128)(2,1)} %get-tuple-element.81.refs_5_), channel_id=1, source_target_pairs={{0,4},{4,0},{1,5},{5,1},{2,6},{6,2},{3,7},{7,3}} | collective-permute-start | bytes 1572872 | tf_op jit(solution)/shard_map/ppermute | solution.py:830
  243.4 77.6 %collective-permute-start.15 = (bf16[2,2,256,256]{3,2,1,0:T(8,128)(2,1)}, bf16[2,2,256,256]{3,2,1,0:T(8,128)(2,1)}, u32[]{:S(2)}, u32[]{:S(2)}) collective-permute-start(bf16[2,2,256,256]{3,2,1,0:T(8,128)(2,1)} %get-tuple-element.85.refs_5_.refs_6_), channel_id=1, source_target_pairs={{0,4},{4,0},{1,5},{5,1},{2,6},{6,2},{3,7},{7,3}} | collective-permute-start | bytes 1572872 | tf_op jit(solution)/shard_map/ppermute | solution.py:830
  251.7 80.1 %collective-permute-start.16 = (bf16[2,2,256,256]{3,2,1,0:T(8,128)(2,1)}, bf16[2,2,256,256]{3,2,1,0:T(8,128)(2,1)}, u32[]{:S(2)}, u32[]{:S(2)}) collective-permute-start(bf16[2,2,256,256]{3,2,1,0:T(8,128)(2,1)} %qkv.10.refs_5_.refs_7_), channel_id=1, source_target_pairs={{0,4},{4,0},{1,5},{5,1},{2,6},{6,2},{3,7},{7,3}} | collective-permute-start | bytes 1572872 | tf_op jit(solution)/shard_map/ppermute | solution.py:830
  287.3 212.5 %collective-permute-start.20 = (bf16[1024,4096]{1,0:T(8,128)(2,1)}, bf16[1024,4096]{1,0:T(8,128)(2,1)}, u32[]{:S(2)}, u32[]{:S(2)}) collective-permute-start(bf16[1024,4096]{1,0:T(8,128)(2,1)} %bitcast.22), channel_id=1, source_target_pairs={{0,1},{1,0},{2,3},{3,2},{4,5},{5,4},{6,7},{7,6}} | collective-permute-start | bytes 25165832 | tf_op jit(solution)/shard_map/ppermute | solution.py:830
  298.5 106.3 %collective-permute-start.21 = (bf16[256,4096]{1,0:T(8,128)(2,1)}, bf16[256,4096]{1,0:T(8,128)(2,1)}, u32[]{:S(2)}, u32[]{:S(2)}) collective-permute-start(bf16[256,4096]{1,0:T(8,128)(2,1)} %get-tuple-element.97), channel_id=1, source_target_pairs={{0,2},{1,3},{2,0},{3,1},{4,6},{5,7},{6,4},{7,5}} | collective-permute-start | bytes 6291464 | tf_op jit(solution)/shard_map/ppermute | solution.py:830
  309.8 95.1 %collective-permute-start.22 = (bf16[256,4096]{1,0:T(8,128)(2,1)}, bf16[256,4096]{1,0:T(8,128)(2,1)}, u32[]{:S(2)}, u32[]{:S(2)}) collective-permute-start(bf16[256,4096]{1,0:T(8,128)(2,1)} %get-tuple-element.99), channel_id=1, source_target_pairs={{0,2},{1,3},{2,0},{3,1},{4,6},{5,7},{6,4},{7,5}} | collective-permute-start | bytes 6291464 | tf_op jit(solution)/shard_map/ppermute | solution.py:830
  404.8 3.0 collective-permute-start.17
  404.9 47.7 %collective-permute-start.18 = (bf16[2,256,1024]{2,1,0:T(8,128)(2,1)}, bf16[2,256,1024]{2,1,0:T(8,128)(2,1)}, u32[]{:S(2)}, u32[]{:S(2)}) collective-permute-start(bf16[2,256,1024]{2,1,0:T(8,128)(2,1)} %get-tuple-element.94), channel_id=1, source_target_pairs={{0,2},{1,3},{2,0},{3,1},{4,6},{5,7},{6,4},{7,5}} | collective-permute-start | bytes 3145736 | tf_op jit(solution)/shard_map/ppermute | solution.py:830
  406.5 46.2 %collective-permute-start.19 = (bf16[2,256,1024]{2,1,0:T(8,128)(2,1)}, bf16[2,256,1024]{2,1,0:T(8,128)(2,1)}, u32[]{:S(2)}, u32[]{:S(2)}) collective-permute-start(bf16[2,256,1024]{2,1,0:T(8,128)(2,1)} %get-tuple-element.95), channel_id=1, source_target_pairs={{0,3},{1,2},{2,1},{3,0},{4,7},{5,6},{6,5},{7,4}} | collective-permute-start | bytes 3145736 | tf_op jit(solution)/shard_map/ppermute | solution.py:830
  406.7 48.8 %collective-permute-start.23 = (bf16[256,4096]{1,0:T(8,128)(2,1)}, bf16[256,4096]{1,0:T(8,128)(2,1)}, u32[]{:S(2)}, u32[]{:S(2)}) collective-permute-start(bf16[256,4096]{1,0:T(8,128)(2,1)} %collective-permute-done.21.refs_6_), channel_id=1, source_target_pairs={{0,4},{4,0},{1,5},{5,1},{2,6},{6,2},{3,7},{7,3}} | collective-permute-start | bytes 6291464 | tf_op jit(solution)/shard_map/ppermute | solution.py:830
  407.8 92.0 %collective-permute-start.24 = (bf16[256,4096]{1,0:T(8,128)(2,1)}, bf16[256,4096]{1,0:T(8,128)(2,1)}, u32[]{:S(2)}, u32[]{:S(2)}) collective-permute-start(bf16[256,4096]{1,0:T(8,128)(2,1)} %collective-permute-done.22.refs_7_), channel_id=1, source_target_pairs={{0,4},{4,0},{1,5},{5,1},{2,6},{6,2},{3,7},{7,3}} | collective-permute-start | bytes 6291464 | tf_op jit(solution)/shard_map/ppermute | solution.py:830
  529.1 47.7 %collective-permute-start.25 = (bf16[256,4096]{1,0:T(8,128)(2,1)}, bf16[256,4096]{1,0:T(8,128)(2,1)}, u32[]{:S(2)}, u32[]{:S(2)}) collective-permute-start(bf16[256,4096]{1,0:T(8,128)(2,1)} %get-tuple-element.104.refs_0_), channel_id=1, source_target_pairs={{0,2},{1,3},{2,0},{3,1},{4,6},{5,7},{6,4},{7,5}} | collective-permute-start | bytes 6291464 | tf_op jit(solution)/shard_map/ppermute | solution.py:830
  574.7 92.6 %collective-permute-start.28 = (bf16[2,256,1024]{2,1,0:T(8,128)(2,1)}, bf16[2,256,1024]{2,1,0:T(8,128)(2,1)}, u32[]{:S(2)}, u32[]{:S(2)}) collective-permute-start(bf16[2,256,1024]{2,1,0:T(8,128)(2,1)} %get-tuple-element.115), channel_id=1, source_target_pairs={{0,1},{1,0},{2,3},{3,2},{4,5},{5,4},{6,7},{7,6}} | collective-permute-start | bytes 3145736 | tf_op jit(solution)/shard_map/ppermute | solution.py:830
  574.7 92.6 %collective-permute-start.29 = (bf16[2,256,1024]{2,1,0:T(8,128)(2,1)}, bf16[2,256,1024]{2,1,0:T(8,128)(2,1)}, u32[]{:S(2)}, u32[]{:S(2)}) collective-permute-start(bf16[2,256,1024]{2,1,0:T(8,128)(2,1)} %get-tuple-element.116), channel_id=1, source_target_pairs={{0,2},{1,3},{2,0},{3,1},{4,6},{5,7},{6,4},{7,5}} | collective-permute-start | bytes 3145736 | tf_op jit(solution)/shard_map/ppermute | solution.py:830
  574.8 92.6 %collective-permute-start.30 = (bf16[2,256,1024]{2,1,0:T(8,128)(2,1)}, bf16[2,256,1024]{2,1,0:T(8,128)(2,1)}, u32[]{:S(2)}, u32[]{:S(2)}) collective-permute-start(bf16[2,256,1024]{2,1,0:T(8,128)(2,1)} %get-tuple-element.117), channel_id=1, source_target_pairs={{0,3},{1,2},{2,1},{3,0},{4,7},{5,6},{6,5},{7,4}} | collective-permute-start | bytes 3145736 | tf_op jit(solution)/shard_map/ppermute | solution.py:830
  576.6 123.9 %collective-permute-start.27 = (bf16[256,4096]{1,0:T(8,128)(2,1)}, bf16[256,4096]{1,0:T(8,128)(2,1)}, u32[]{:S(2)}, u32[]{:S(2)}) collective-permute-start(bf16[256,4096]{1,0:T(8,128)(2,1)} %get-tuple-element.113.refs_0_), channel_id=1, source_target_pairs={{0,2},{1,3},{2,0},{3,1},{4,6},{5,7},{6,4},{7,5}} | collective-permute-start | bytes 6291464 | tf_op jit(solution)/shard_map/ppermute | solution.py:830
  696.7 143.7 %collective-permute-start.32 = (bf16[256,4096]{1,0:T(8,128)(2,1)}, bf16[256,4096]{1,0:T(8,128)(2,1)}, u32[]{:S(2)}, u32[]{:S(2)}) collective-permute-start(bf16[256,4096]{1,0:T(8,128)(2,1)} %get-tuple-element.122.refs_0_), channel_id=1, source_target_pairs={{0,2},{1,3},{2,0},{3,1},{4,6},{5,7},{6,4},{7,5}} | collective-permute-start | bytes 6291464 | tf_op jit(solution)/shard_map/ppermute | solution.py:830
  698.4 239.0 %collective-permute-start.34 = (bf16[256,4096]{1,0:T(8,128)(2,1)}, bf16[256,4096]{1,0:T(8,128)(2,1)}, u32[]{:S(2)}, u32[]{:S(2)}) collective-permute-start(bf16[256,4096]{1,0:T(8,128)(2,1)} %get-tuple-element.125.refs_0_), channel_id=1, source_target_pairs={{0,2},{1,3},{2,0},{3,1},{4,6},{5,7},{6,4},{7,5}} | collective-permute-start | bytes 6291464 | tf_op jit(solution)/shard_map/ppermute | solution.py:830
  698.7 136.7 %collective-permute-start.26 = (bf16[256,4096]{1,0:T(8,128)(2,1)}, bf16[256,4096]{1,0:T(8,128)(2,1)}, u32[]{:S(2)}, u32[]{:S(2)}) collective-permute-start(bf16[256,4096]{1,0:T(8,128)(2,1)} %get-tuple-element.112), channel_id=1, source_target_pairs={{0,2},{1,3},{2,0},{3,1},{4,6},{5,7},{6,4},{7,5}} | collective-permute-start | bytes 6291464 | tf_op jit(solution)/shard_map/ppermute | solution.py:830
  791.0 141.5 %collective-permute-start.31 = (bf16[256,4096]{1,0:T(8,128)(2,1)}, bf16[256,4096]{1,0:T(8,128)(2,1)}, u32[]{:S(2)}, u32[]{:S(2)}) collective-permute-start(bf16[256,4096]{1,0:T(8,128)(2,1)} %get-tuple-element.120), channel_id=1, source_target_pairs={{0,2},{1,3},{2,0},{3,1},{4,6},{5,7},{6,4},{7,5}} | collective-permute-start | bytes 6291464 | tf_op jit(solution)/shard_map/ppermute | solution.py:830
  930.8 56.7 %collective-permute-start.33 = (bf16[256,4096]{1,0:T(8,128)(2,1)}, bf16[256,4096]{1,0:T(8,128)(2,1)}, u32[]{:S(2)}, u32[]{:S(2)}) collective-permute-start(bf16[256,4096]{1,0:T(8,128)(2,1)} %get-tuple-element.124), channel_id=1, source_target_pairs={{0,2},{1,3},{2,0},{3,1},{4,6},{5,7},{6,4},{7,5}} | collective-permute-start | bytes 6291464 | tf_op jit(solution)/shard_map/ppermute | solution.py:830
  987.1 67.1 %collective-permute-start.35 = (bf16[128,4096]{1,0:T(8,128)(2,1)}, bf16[128,4096]{1,0:T(8,128)(2,1)}, u32[]{:S(2)}, u32[]{:S(2)}) collective-permute-start(bf16[128,4096]{1,0:T(8,128)(2,1)} %get-tuple-element.127), channel_id=1, source_target_pairs={{0,2},{1,3},{2,0},{3,1},{4,6},{5,7},{6,4},{7,5}} | collective-permute-start | bytes 3145736 | tf_op jit(solution)/shard_map/ppermute | solution.py:830

commit v18 on v16

--- a/solution.py
+++ b/solution.py
@@ -419,7 +419,9 @@
                             pltpu.SemaphoreType.DMA((n_tiles,)), *scratch]),
         out_shape=out_shape,
         input_output_aliases={n_in - len(old) + k: k for k in range(len(old))},
-        name="flash" if final else "flash_part", compiler_params=PARAMS,
+        name="flash" if final else "flash_part",
+        compiler_params=pltpu.CompilerParams(
+            vmem_limit_bytes=VMEM),
         cost_estimate=cost(8 * work * RUN * RUN * nq, n_runs * RUN * nq),
     )(tab, *qs, *kvs, *sts, *more, *after)
 
@@ -498,7 +500,7 @@
     lax.fori_loop(0, len(loads), one, 0)
     x_copy.wait()
 
-    strip = 32
+    strip = 64
 
     def one_strip(r, carry):
         rows = pl.ds(pl.multiple_of(r * strip, strip), strip)
@@ -507,12 +509,15 @@
         o_scr[rows, :] = norm_rows(y, g_ref[:])
         return carry
 
-    stores, per = [], RUN // strip
+    stores, part = [], RUN // 2
     for i in range(n_run):
-        lax.fori_loop(i * per, (i + 1) * per, one_strip, 0)
-        for k, scr in enumerate((x_scr, o_scr)):
-            stores.append(pltpu.make_async_copy(scr.at[pl.ds(i * RUN, RUN), :], outs[2 * i + k], out_sem.at[2 * i + k]))
-            stores[-1].start()
+        for h in PAIR:
+            r0 = i * RUN + h * part
+            lax.fori_loop(r0 // strip, (r0 + part) // strip, one_strip, 0)
+            for k, scr in enumerate((x_scr, o_scr)):
+                stores.append(pltpu.make_async_copy(scr.at[pl.ds(r0, part), :], outs[2 * i + k].at[pl.ds(h * part, part), :],
+                                                    out_sem.at[len(stores)]))
+                stores[-1].start()
     for cp in stores:
         cp.wait()
     for cp in shared:
@@ -532,7 +537,7 @@
         out_shape=[jax.ShapeDtypeStruct((RUN, dim), BF)] * (2 * n_run),
         scratch_shapes=[pltpu.VMEM((rows, 4 * width), BF), pltpu.VMEM((3 + n_shared, width // 2, dim), BF), pltpu.VMEM((rows, dim), BF),
                         pltpu.VMEM((rows, dim), F32), pltpu.SemaphoreType.DMA((len(blocks) + n_shared, 2 * n_run)),
-                        pltpu.SemaphoreType.DMA((3 + n_shared,)), pltpu.SemaphoreType.DMA, pltpu.SemaphoreType.DMA((2 * n_run,)),
+                        pltpu.SemaphoreType.DMA((3 + n_shared,)), pltpu.SemaphoreType.DMA, pltpu.SemaphoreType.DMA((4 * n_run,)),
                         pltpu.SemaphoreType.DMA((len(ws),))],
         name="outp",
         compiler_params=pltpu.CompilerParams(vmem_limit_bytes=VMEM, collective_id=call, has_side_effects=True),

time: 1070 us -> 1060 us (level)
  no operation moved by 1% of the time
where the time goes in v18:
time: 1060 us
  Pallas kernels  777 us (73%)
  waiting for transfers between devices  223 us (21%)
  starting transfers between devices  28.2 us (3%)
  local copies, waits for them, and re-layouts  18.8 us (2%)
    pallas_call x5, Pallas kernels, mlp(): pl.pallas_call(ordered(functools.partial(mlp_kernel, n_in=len(bs), first=...  383 us
    ppermute x36, waiting for transfers between devices, send(): return lax.ppermute(v, *axis_pairs)  223 us
    pallas_call x5, Pallas kernels, flash(): pl.pallas_call(ordered(functools.partial(flash_kernel, q_src=q_src, kv_sr...  211 us
    pallas_call x6, Pallas kernels, qkv(): pl.pallas_call(ordered(functools.partial(qkv_kernel, n_in=n_in, n_q=n_q,...  97.6 us
    pallas_call x2, Pallas kernels, out_proj(): pl.pallas_call(ordered(functools.partial(out_kernel, blocks=blocks, n_w=l...  53.9 us
    ppermute x36, starting transfers between devices, send(): return lax.ppermute(v, *axis_pairs)  28.2 us
  transfers between devices with their start and end apart: 36, of which 15 were waited for; matrix products, arithmetic and copies ran while one was open for 2% of the time, Pallas kernels for 70%

profile of v18, /device:TPU:0, one launch (start us, length us, event | category | flops | bytes accessed | tf_op | source)
XLA Modules:
  0.0 1055.1 jit_solution(18084047572854465232)
XLA Ops:
  1.3 3.4 norm.2.refs_2_.refs_0_
  4.7 3.3 collective-permute-start.5
  8.0 8.6 norm.3
  19.1 9.5 bitcast_dynamic-update-slice_fusion
  28.6 2.8 multiply_sine_fusion.1
  31.4 2.0 bitcast_dynamic-update-slice_fusion.2
  33.4 2.0 bitcast_dynamic-update-slice_fusion.1.refs_8_.refs_2_
  35.4 37.6 %qkv.6 = (bf16[8,1024,256]{2,1,0:T(8,128)(2,1)}, bf16[8,2,256,256]{3,2,1,0:T(8,128)(2,1)}) custom-call(bf16[256,4096]{1,0:T(8,128)(2,1)} %norm.2.refs_2_.refs_0_, bf16[256,4096]{1,0:T(8,128)(2,1)} %get-tuple-element.67.refs_1_, bf16[256,4096]{1,0:T(8,128)(2,1)} %get-tuple-element.68.refs_2_, bf16[256,4096]{1,0:T(8,128)(2,1)} %get-tuple-element.69.refs_3_, ...), custom_call_target="tpu_custom_call" | custom-call | flops 25769803776 | bytes 12582912 | tf_op jit(solution)/shard_map/qkv/pallas_call | solution.py:139
  73.8 3.4 multiply_sine_fusion
  77.6 14.0 %qkv.7 = (bf16[2,1024,256]{2,1,0:T(8,128)(2,1)}, bf16[2,2,256,256]{3,2,1,0:T(8,128)(2,1)}) custom-call(bf16[256,4096]{1,0:T(8,128)(2,1)} %collective-permute-done.5.refs_0_, bf16[256,4096]{1,0:T(8,128)(2,1)} %collective-permute-done.6.refs_1_, bf16[4096,1536]{1,0:T(8,128)(2,1)} %bitcast_dynamic-update-slice_fusion.1.refs_8_.refs_2_, ...), custom_call_target="tpu_custom_call" | custom-call | flops 6442450944 | bytes 12582912 | tf_op jit(solution)/shard_map/qkv/pallas_call | solution.py:139
  91.6 29.8 %collective-permute-done.4.refs_0_ = bf16[256,4096]{1,0:T(8,128)(2,1)} collective-permute-done((bf16[256,4096]{1,0:T(8,128)(2,1)}, bf16[256,4096]{1,0:T(8,128)(2,1)}, u32[]{:S(2)}, u32[]{:S(2)}) %collective-permute-start.4) | collective-permute-done | bytes 2097184 | tf_op jit(solution)/shard_map/ppermute | solution.py:833
  123.1 2.9 collective-permute-done.7.refs_1_
  126.0 13.6 %qkv.8 = (bf16[2,1024,256]{2,1,0:T(8,128)(2,1)}, bf16[2,2,256,256]{3,2,1,0:T(8,128)(2,1)}) custom-call(bf16[256,4096]{1,0:T(8,128)(2,1)} %collective-permute-done.4.refs_0_, bf16[256,4096]{1,0:T(8,128)(2,1)} %collective-permute-done.7.refs_1_, bf16[4096,1536]{1,0:T(8,128)(2,1)} %bitcast_dynamic-update-slice_fusion.1.refs_8_.refs_2_, ...), custom_call_target="tpu_custom_call" | custom-call | flops 6442450944 | bytes 12582912 | tf_op jit(solution)/shard_map/qkv/pallas_call | solution.py:139
  139.5 50.0 %flash_part.1 = (f32[10,2,4,144,256]{4,3,2,1,0:T(8,128)}, bf16[256,4096]{1,0:T(8,128)(2,1)}, bf16[256,4096]{1,0:T(8,128)(2,1)}) custom-call(s32[845]{0:T(1024)} %dynamic-slice_reduce_fusion.refs_0_, bf16[8,1024,256]{2,1,0:T(8,128)(2,1)} %get-tuple-element.74.refs_1_, bf16[2,1024,256]{2,1,0:T(8,128)(2,1)} %get-tuple-element.82.refs_2_, ...), custom_call_target="tpu_custom_call" | custom-call | flops 38654705664 | bytes 3145728 | tf_op jit(solution)/shard_map/flash_part/pallas_call | solution.py:398
  191.7 3.0 collective-permute-done.9.refs_1_
  194.7 13.7 %qkv.9 = (bf16[2,1024,256]{2,1,0:T(8,128)(2,1)}, bf16[2,2,256,256]{3,2,1,0:T(8,128)(2,1)}) custom-call(bf16[256,4096]{1,0:T(8,128)(2,1)} %collective-permute-done.8.refs_0_, bf16[256,4096]{1,0:T(8,128)(2,1)} %collective-permute-done.9.refs_1_, bf16[4096,1536]{1,0:T(8,128)(2,1)} %bitcast_dynamic-update-slice_fusion.1.refs_8_.refs_2_, ...), custom_call_target="tpu_custom_call" | custom-call | flops 6442450944 | bytes 12582912 | tf_op jit(solution)/shard_map/qkv/pallas_call | solution.py:139
  208.5 30.0 %collective-permute-done.10.refs_0_ = bf16[256,4096]{1,0:T(8,128)(2,1)} collective-permute-done((bf16[256,4096]{1,0:T(8,128)(2,1)}, bf16[256,4096]{1,0:T(8,128)(2,1)}, u32[]{:S(2)}, u32[]{:S(2)}) %collective-permute-start.10) | collective-permute-done | bytes 2097184 | tf_op jit(solution)/shard_map/ppermute | solution.py:833
  243.8 7.8 qkv.10.refs_5_.refs_7_
  253.2 10.8 %qkv.11.refs_14_.refs_2_ = bf16[2,1024,256]{2,1,0:T(8,128)(2,1)} custom-call(bf16[256,4096]{1,0:T(8,128)(2,1)} %collective-permute-done.10.refs_0_, bf16[256,4096]{1,0:T(8,128)(2,1)} %collective-permute-done.11.refs_1_, bf16[4096,1536]{1,0:T(8,128)(2,1)} %bitcast_dynamic-update-slice_fusion.1.refs_8_.refs_2_, f32[8,64,256]{2,1,0:T(8,128)} %get-tuple-element.132.refs_3_, ...), custom_call_target="tpu_custom_call" | custom-call | flops 6442450944 | bytes 12582912 | tf_op jit(solution)/shard_map/qkv/pallas_call | solution.py:139
  264.0 23.3 %collective-permute-done.12.refs_8_ = bf16[8,2,256,256]{3,2,1,0:T(8,128)(2,1)} collective-permute-done((bf16[8,2,256,256]{3,2,1,0:T(8,128)(2,1)}, bf16[8,2,256,256]{3,2,1,0:T(8,128)(2,1)}, u32[]{:S(2)}, u32[]{:S(2)}) %collective-permute-start.12) | collective-permute-done | bytes 2097184 | tf_op jit(solution)/shard_map/ppermute | solution.py:833
  287.3 11.2 %collective-permute-done.13.refs_9_ = bf16[2,2,256,256]{3,2,1,0:T(8,128)(2,1)} collective-permute-done((bf16[2,2,256,256]{3,2,1,0:T(8,128)(2,1)}, bf16[2,2,256,256]{3,2,1,0:T(8,128)(2,1)}, u32[]{:S(2)}, u32[]{:S(2)}) %collective-permute-start.13) | collective-permute-done | bytes 524320 | tf_op jit(solution)/shard_map/ppermute | solution.py:833
  300.1 9.7 collective-permute-done.14.refs_10_
  311.3 9.7 collective-permute-done.15.refs_11_
  321.0 10.8 %collective-permute-done.16.refs_12_ = bf16[2,2,256,256]{3,2,1,0:T(8,128)(2,1)} collective-permute-done((bf16[2,2,256,256]{3,2,1,0:T(8,128)(2,1)}, bf16[2,2,256,256]{3,2,1,0:T(8,128)(2,1)}, u32[]{:S(2)}, u32[]{:S(2)}) %collective-permute-start.16) | collective-permute-done | bytes 524320 | tf_op jit(solution)/shard_map/ppermute | solution.py:833
  331.8 29.1 %flash.4 = (bf16[2,256,1024]{2,1,0:T(8,128)(2,1)}, bf16[2,256,1024]{2,1,0:T(8,128)(2,1)}, bf16[2,256,1024]{2,1,0:T(8,128)(2,1)}, bf16[2,256,1024]{2,1,0:T(8,128)(2,1)}, f32[8,128]{1,0:T(8,128)}) custom-call(s32[845]{0:T(1024)} %dynamic-slice_reduce_fusion.refs_0_, bf16[8,1024,256]{2,1,0:T(8,128)(2,1)} %get-tuple-element.74.refs_1_, ...), custom_call_target="tpu_custom_call" | custom-call | flops 23622320128 | bytes 8388608 | tf_op jit(solution)/shard_map/flash/pallas_call | solution.py:398
  360.9 43.9 %flash.5 = (bf16[2,256,1024]{2,1,0:T(8,128)(2,1)}, bf16[2,256,1024]{2,1,0:T(8,128)(2,1)}, bf16[2,256,1024]{2,1,0:T(8,128)(2,1)}, bf16[2,256,1024]{2,1,0:T(8,128)(2,1)}, f32[8,128]{1,0:T(8,128)}) custom-call(s32[845]{0:T(1024)} %dynamic-slice_reduce_fusion.refs_0_, ...), custom_call_target="tpu_custom_call", output_to_operand_aliasing={{0}: (14, {}), {1}: (15, {}), {2}: (16, {}), {3}: (17, {})} | custom-call | flops 32212254720 | bytes 8388608 | tf_op jit(solution)/shard_map/flash/pallas_call | solution.py:398
  404.9 1.7 collective-permute-start.18
  408.7 43.8 %flash.6 = (bf16[2,256,1024]{2,1,0:T(8,128)(2,1)}, bf16[2,256,1024]{2,1,0:T(8,128)(2,1)}, bf16[2,256,1024]{2,1,0:T(8,128)(2,1)}, bf16[2,256,1024]{2,1,0:T(8,128)(2,1)}, f32[8,128]{1,0:T(8,128)}) custom-call(s32[845]{0:T(1024)} %dynamic-slice_reduce_fusion.refs_0_, bf16[8,1024,256]{2,1,0:T(8,128)(2,1)} %get-tuple-element.74.refs_1_, ...), custom_call_target="tpu_custom_call" | custom-call | flops 32212254720 | bytes 8388608 | tf_op jit(solution)/shard_map/flash/pallas_call | solution.py:398
  452.7 2.8 collective-permute-done.23.refs_8_
  455.5 44.3 %collective-permute-done.24.refs_9_ = bf16[256,4096]{1,0:T(8,128)(2,1)} collective-permute-done((bf16[256,4096]{1,0:T(8,128)(2,1)}, bf16[256,4096]{1,0:T(8,128)(2,1)}, u32[]{:S(2)}, u32[]{:S(2)}) %collective-permute-start.24) | collective-permute-done | bytes 2097184 | tf_op jit(solution)/shard_map/ppermute | solution.py:833
  499.8 26.9 %outp.2 = (bf16[256,4096]{1,0:T(8,128)(2,1)}, bf16[256,4096]{1,0:T(8,128)(2,1)}, bf16[256,4096]{1,0:T(8,128)(2,1)}, bf16[256,4096]{1,0:T(8,128)(2,1)}) custom-call(bf16[2,256,1024]{2,1,0:T(8,128)(2,1)} %get-tuple-element.92.refs_0_, bf16[2,256,1024]{2,1,0:T(8,128)(2,1)} %collective-permute-done.17.refs_1_, ...), custom_call_target="tpu_custom_call" | custom-call | flops 17179869184 | bytes 33554432 | tf_op jit(solution)/shard_map/outp/pallas_call | solution.py:531
  528.4 43.9 %flash.7 = (bf16[2,256,1024]{2,1,0:T(8,128)(2,1)}, bf16[2,256,1024]{2,1,0:T(8,128)(2,1)}, bf16[2,256,1024]{2,1,0:T(8,128)(2,1)}, bf16[2,256,1024]{2,1,0:T(8,128)(2,1)}, f32[8,128]{1,0:T(8,128)}) custom-call(s32[845]{0:T(1024)} %dynamic-slice_reduce_fusion.refs_0_, ...), custom_call_target="tpu_custom_call", output_to_operand_aliasing={{0}: (14, {}), {1}: (15, {}), {2}: (16, {}), {3}: (17, {})} | custom-call | flops 32212254720 | bytes 8388608 | tf_op jit(solution)/shard_map/flash/pallas_call | solution.py:398
  572.4 1.8 collective-permute-start.30
  574.5 90.4 %mlp.5 = (bf16[256,4096]{1,0:T(8,128)(2,1)}, bf16[256,4096]{1,0:T(8,128)(2,1)}) custom-call(bf16[256,4096]{1,0:T(8,128)(2,1)} %get-tuple-element.104.refs_0_, bf16[256,4096]{1,0:T(8,128)(2,1)} %collective-permute-done.25.refs_1_, bf16[4096,3072]{1,0:T(8,128)(2,1)} %refs_2_.9, bf16[4096,3072]{1,0:T(8,128)(2,1)} %refs_3_.9, bf16[3072,4096]{1,0:T(8,128)(2,1)} %refs_4_.9, ...), custom_call_target="tpu_custom_call" | custom-call | flops 77309411328 | bytes 75497472 | tf_op jit(solution)/shard_map/mlp/pallas_call | solution.py:693
  665.0 27.0 %outp.3 = (bf16[256,4096]{1,0:T(8,128)(2,1)}, bf16[256,4096]{1,0:T(8,128)(2,1)}, bf16[256,4096]{1,0:T(8,128)(2,1)}, bf16[256,4096]{1,0:T(8,128)(2,1)}) custom-call(bf16[2,256,1024]{2,1,0:T(8,128)(2,1)} %get-tuple-element.114.refs_0_, bf16[2,256,1024]{2,1,0:T(8,128)(2,1)} %collective-permute-done.28.refs_1_, ...), custom_call_target="tpu_custom_call" | custom-call | flops 17179869184 | bytes 33554432 | tf_op jit(solution)/shard_map/outp/pallas_call | solution.py:531
  691.9 1.7 collective-permute-start.32
  694.0 1.7 collective-permute-start.26
  695.7 90.6 %mlp.6 = (bf16[256,4096]{1,0:T(8,128)(2,1)}, bf16[256,4096]{1,0:T(8,128)(2,1)}) custom-call(bf16[256,4096]{1,0:T(8,128)(2,1)} %get-tuple-element.113.refs_0_, bf16[256,4096]{1,0:T(8,128)(2,1)} %collective-permute-done.27.refs_1_, bf16[4096,3072]{1,0:T(8,128)(2,1)} %refs_2_.9, bf16[4096,3072]{1,0:T(8,128)(2,1)} %refs_3_.9, bf16[3072,4096]{1,0:T(8,128)(2,1)} %refs_4_.9, ...), custom_call_target="tpu_custom_call" | custom-call | flops 77309411328 | bytes 75497472 | tf_op jit(solution)/shard_map/mlp/pallas_call | solution.py:693
  786.6 44.1 %collective-permute-done.26.refs_1_ = bf16[256,4096]{1,0:T(8,128)(2,1)} collective-permute-done((bf16[256,4096]{1,0:T(8,128)(2,1)}, bf16[256,4096]{1,0:T(8,128)(2,1)}, u32[]{:S(2)}, u32[]{:S(2)}) %collective-permute-start.26) | collective-permute-done | bytes 2097184 | tf_op jit(solution)/shard_map/ppermute | solution.py:833
  830.7 4.9 zsum.5.refs_5_.refs_0_
  835.6 90.4 %mlp.7 = (bf16[256,4096]{1,0:T(8,128)(2,1)}, bf16[256,4096]{1,0:T(8,128)(2,1)}) custom-call(bf16[256,4096]{1,0:T(8,128)(2,1)} %get-tuple-element.122.refs_0_, bf16[256,4096]{1,0:T(8,128)(2,1)} %collective-permute-done.32.refs_1_, bf16[4096,3072]{1,0:T(8,128)(2,1)} %refs_2_.9, bf16[4096,3072]{1,0:T(8,128)(2,1)} %refs_3_.9, bf16[3072,4096]{1,0:T(8,128)(2,1)} %refs_4_.9, ...), custom_call_target="tpu_custom_call" | custom-call | flops 77309411328 | bytes 75497472 | tf_op jit(solution)/shard_map/mlp/pallas_call | solution.py:693
  926.0 1.7 collective-permute-start.33
  927.8 4.9 zsum.6.refs_5_.refs_0_
  932.7 49.7 %mlp.8 = (bf16[128,4096]{1,0:T(8,128)(2,1)}, bf16[128,4096]{1,0:T(8,128)(2,1)}) custom-call(bf16[256,4096]{1,0:T(8,128)(2,1)} %get-tuple-element.125.refs_0_, bf16[256,4096]{1,0:T(8,128)(2,1)} %collective-permute-done.34.refs_1_, bf16[4096,3072]{1,0:T(8,128)(2,1)} %refs_2_.9, bf16[4096,3072]{1,0:T(8,128)(2,1)} %refs_3_.9, bf16[3072,4096]{1,0:T(8,128)(2,1)} %refs_4_.9, ...), custom_call_target="tpu_custom_call" | custom-call | flops 38654705664 | bytes 75497472 | tf_op jit(solution)/shard_map/mlp/pallas_call | solution.py:693
  982.8 4.9 zsum.7.refs_5_.refs_0_
  987.7 61.8 %mlp.9.refs_4_.refs_1_ = bf16[128,4096]{1,0:T(8,128)(2,1)} custom-call(bf16[256,4096]{1,0:T(8,128)(2,1)} %get-tuple-element.125.refs_0_, bf16[256,4096]{1,0:T(8,128)(2,1)} %collective-permute-done.34.refs_1_, bf16[4096,3072]{1,0:T(8,128)(2,1)} %refs_2_.9, bf16[4096,3072]{1,0:T(8,128)(2,1)} %refs_3_.9, bf16[3072,4096]{1,0:T(8,128)(2,1)} %refs_4_.9, ...), custom_call_target="tpu_custom_call" | custom-call | flops 38654705664 | bytes 75497472 | tf_op jit(solution)/shard_map/mlp/pallas_call | solution.py:693
  1049.5 2.9 zsum.8.refs_0_
  1052.4 2.4 zsum.9
  (69 shorter events, 23.9 us)
Async XLA Ops:
  4.7 68.3 %collective-permute-start.5 = (bf16[256,4096]{1,0:T(8,128)(2,1)}, bf16[256,4096]{1,0:T(8,128)(2,1)}, u32[]{:S(2)}, u32[]{:S(2)}) collective-permute-start(bf16[256,4096]{1,0:T(8,128)(2,1)} %norm.2.refs_2_.refs_0_), channel_id=1, source_target_pairs={{0,2},{1,3},{2,0},{3,1},{4,6},{5,7},{6,4},{7,5}} | collective-permute-start | bytes 6291464 | tf_op jit(solution)/shard_map/ppermute | solution.py:833
  8.0 27.4 %collective-permute-start = (bf16[256,4096]{1,0:T(8,128)(2,1)}, bf16[256,4096]{1,0:T(8,128)(2,1)}, u32[]{:S(2)}, u32[]{:S(2)}) collective-permute-start(bf16[256,4096]{1,0:T(8,128)(2,1)} %norm.2.refs_2_.refs_0_), channel_id=1, source_target_pairs={{0,1},{1,0},{2,3},{3,2},{4,5},{5,4},{6,7},{7,6}} | collective-permute-start | bytes 6291464 | tf_op jit(solution)/shard_map/ppermute | solution.py:833
  16.7 18.7 %collective-permute-start.1 = (bf16[256,4096]{1,0:T(8,128)(2,1)}, bf16[256,4096]{1,0:T(8,128)(2,1)}, u32[]{:S(2)}, u32[]{:S(2)}) collective-permute-start(bf16[256,4096]{1,0:T(8,128)(2,1)} %get-tuple-element.67.refs_1_), channel_id=1, source_target_pairs={{0,1},{1,0},{2,3},{3,2},{4,5},{5,4},{6,7},{7,6}} | collective-permute-start | bytes 6291464 | tf_op jit(solution)/shard_map/ppermute | solution.py:833
  17.2 18.2 %collective-permute-start.2 = (bf16[256,4096]{1,0:T(8,128)(2,1)}, bf16[256,4096]{1,0:T(8,128)(2,1)}, u32[]{:S(2)}, u32[]{:S(2)}) collective-permute-start(bf16[256,4096]{1,0:T(8,128)(2,1)} %get-tuple-element.68.refs_2_), channel_id=1, source_target_pairs={{0,1},{1,0},{2,3},{3,2},{4,5},{5,4},{6,7},{7,6}} | collective-permute-start | bytes 6291464 | tf_op jit(solution)/shard_map/ppermute | solution.py:833
  17.2 18.2 %collective-permute-start.3 = (bf16[256,4096]{1,0:T(8,128)(2,1)}, bf16[256,4096]{1,0:T(8,128)(2,1)}, u32[]{:S(2)}, u32[]{:S(2)}) collective-permute-start(bf16[256,4096]{1,0:T(8,128)(2,1)} %get-tuple-element.69.refs_3_), channel_id=1, source_target_pairs={{0,1},{1,0},{2,3},{3,2},{4,5},{5,4},{6,7},{7,6}} | collective-permute-start | bytes 6291464 | tf_op jit(solution)/shard_map/ppermute | solution.py:833
  17.7 10.9 %copy-start.2 = (f32[64]{0:T(128)}, f32[64]{0:T(128)S(1)}, u32[]{:S(2)}) copy-start(f32[64]{0:T(128)S(1)} %multiply_power_fusion) | copy-start | bytes 772
  19.1 12.3 %copy-start = (bf16[4096,2,128]{2,1,0:T(2,128)(2,1)S(1)}, bf16[4096,2,128]{2,1,0:T(2,128)(2,1)}, u32[]{:S(2)}) copy-start(bf16[4096,2,128]{2,1,0:T(2,128)(2,1)} %param.15) | copy-start | bytes 6291460
  31.4 2.0 copy-start.1
  73.1 4.5 collective-permute-start.6
  73.1 48.3 %collective-permute-start.4 = (bf16[256,4096]{1,0:T(8,128)(2,1)}, bf16[256,4096]{1,0:T(8,128)(2,1)}, u32[]{:S(2)}, u32[]{:S(2)}) collective-permute-start(bf16[256,4096]{1,0:T(8,128)(2,1)} %get-tuple-element.67.refs_1_), channel_id=1, source_target_pairs={{0,2},{1,3},{2,0},{3,1},{4,6},{5,7},{6,4},{7,5}} | collective-permute-start | bytes 6291464 | tf_op jit(solution)/shard_map/ppermute | solution.py:833
  121.4 4.5 collective-permute-start.7
  121.5 68.1 %collective-permute-start.8 = (bf16[256,4096]{1,0:T(8,128)(2,1)}, bf16[256,4096]{1,0:T(8,128)(2,1)}, u32[]{:S(2)}, u32[]{:S(2)}) collective-permute-start(bf16[256,4096]{1,0:T(8,128)(2,1)} %get-tuple-element.68.refs_2_), channel_id=1, source_target_pairs={{0,2},{1,3},{2,0},{3,1},{4,6},{5,7},{6,4},{7,5}} | collective-permute-start | bytes 6291464 | tf_op jit(solution)/shard_map/ppermute | solution.py:833
  189.6 5.1 collective-permute-start.9
  190.6 47.9 %collective-permute-start.10 = (bf16[256,4096]{1,0:T(8,128)(2,1)}, bf16[256,4096]{1,0:T(8,128)(2,1)}, u32[]{:S(2)}, u32[]{:S(2)}) collective-permute-start(bf16[256,4096]{1,0:T(8,128)(2,1)} %get-tuple-element.69.refs_3_), channel_id=1, source_target_pairs={{0,2},{1,3},{2,0},{3,1},{4,6},{5,7},{6,4},{7,5}} | collective-permute-start | bytes 6291464 | tf_op jit(solution)/shard_map/ppermute | solution.py:833
  238.5 5.4 collective-permute-start.11
  238.5 48.8 %collective-permute-start.12 = (bf16[8,2,256,256]{3,2,1,0:T(8,128)(2,1)}, bf16[8,2,256,256]{3,2,1,0:T(8,128)(2,1)}, u32[]{:S(2)}, u32[]{:S(2)}) collective-permute-start(bf16[8,2,256,256]{3,2,1,0:T(8,128)(2,1)} %get-tuple-element.75.refs_5_.refs_3_), channel_id=1, source_target_pairs={{0,4},{4,0},{1,5},{5,1},{2,6},{6,2},{3,7},{7,3}} | collective-permute-start | bytes 6291464 | tf_op jit(solution)/shard_map/ppermute | solution.py:833
  241.3 57.2 %collective-permute-start.13 = (bf16[2,2,256,256]{3,2,1,0:T(8,128)(2,1)}, bf16[2,2,256,256]{3,2,1,0:T(8,128)(2,1)}, u32[]{:S(2)}, u32[]{:S(2)}) collective-permute-start(bf16[2,2,256,256]{3,2,1,0:T(8,128)(2,1)} %get-tuple-element.78.refs_5_.refs_4_), channel_id=1, source_target_pairs={{0,4},{4,0},{1,5},{5,1},{2,6},{6,2},{3,7},{7,3}} | collective-permute-start | bytes 1572872 | tf_op jit(solution)/shard_map/ppermute | solution.py:833
  241.8 68.0 %collective-permute-start.14 = (bf16[2,2,256,256]{3,2,1,0:T(8,128)(2,1)}, bf16[2,2,256,256]{3,2,1,0:T(8,128)(2,1)}, u32[]{:S(2)}, u32[]{:S(2)}) collective-permute-start(bf16[2,2,256,256]{3,2,1,0:T(8,128)(2,1)} %get-tuple-element.81.refs_5_), channel_id=1, source_target_pairs={{0,4},{4,0},{1,5},{5,1},{2,6},{6,2},{3,7},{7,3}} | collective-permute-start | bytes 1572872 | tf_op jit(solution)/shard_map/ppermute | solution.py:833
  243.4 77.6 %collective-permute-start.15 = (bf16[2,2,256,256]{3,2,1,0:T(8,128)(2,1)}, bf16[2,2,256,256]{3,2,1,0:T(8,128)(2,1)}, u32[]{:S(2)}, u32[]{:S(2)}) collective-permute-start(bf16[2,2,256,256]{3,2,1,0:T(8,128)(2,1)} %get-tuple-element.85.refs_5_.refs_6_), channel_id=1, source_target_pairs={{0,4},{4,0},{1,5},{5,1},{2,6},{6,2},{3,7},{7,3}} | collective-permute-start | bytes 1572872 | tf_op jit(solution)/shard_map/ppermute | solution.py:833
  251.7 80.1 %collective-permute-start.16 = (bf16[2,2,256,256]{3,2,1,0:T(8,128)(2,1)}, bf16[2,2,256,256]{3,2,1,0:T(8,128)(2,1)}, u32[]{:S(2)}, u32[]{:S(2)}) collective-permute-start(bf16[2,2,256,256]{3,2,1,0:T(8,128)(2,1)} %qkv.10.refs_5_.refs_7_), channel_id=1, source_target_pairs={{0,4},{4,0},{1,5},{5,1},{2,6},{6,2},{3,7},{7,3}} | collective-permute-start | bytes 1572872 | tf_op jit(solution)/shard_map/ppermute | solution.py:833
  287.3 212.5 %collective-permute-start.20 = (bf16[1024,4096]{1,0:T(8,128)(2,1)}, bf16[1024,4096]{1,0:T(8,128)(2,1)}, u32[]{:S(2)}, u32[]{:S(2)}) collective-permute-start(bf16[1024,4096]{1,0:T(8,128)(2,1)} %bitcast.22), channel_id=1, source_target_pairs={{0,1},{1,0},{2,3},{3,2},{4,5},{5,4},{6,7},{7,6}} | collective-permute-start | bytes 25165832 | tf_op jit(solution)/shard_map/ppermute | solution.py:833
  298.5 106.3 %collective-permute-start.21 = (bf16[256,4096]{1,0:T(8,128)(2,1)}, bf16[256,4096]{1,0:T(8,128)(2,1)}, u32[]{:S(2)}, u32[]{:S(2)}) collective-permute-start(bf16[256,4096]{1,0:T(8,128)(2,1)} %get-tuple-element.97), channel_id=1, source_target_pairs={{0,2},{1,3},{2,0},{3,1},{4,6},{5,7},{6,4},{7,5}} | collective-permute-start | bytes 6291464 | tf_op jit(solution)/shard_map/ppermute | solution.py:833
  309.8 95.1 %collective-permute-start.22 = (bf16[256,4096]{1,0:T(8,128)(2,1)}, bf16[256,4096]{1,0:T(8,128)(2,1)}, u32[]{:S(2)}, u32[]{:S(2)}) collective-permute-start(bf16[256,4096]{1,0:T(8,128)(2,1)} %get-tuple-element.99), channel_id=1, source_target_pairs={{0,2},{1,3},{2,0},{3,1},{4,6},{5,7},{6,4},{7,5}} | collective-permute-start | bytes 6291464 | tf_op jit(solution)/shard_map/ppermute | solution.py:833
  404.8 3.0 collective-permute-start.17
  404.9 47.7 %collective-permute-start.18 = (bf16[2,256,1024]{2,1,0:T(8,128)(2,1)}, bf16[2,256,1024]{2,1,0:T(8,128)(2,1)}, u32[]{:S(2)}, u32[]{:S(2)}) collective-permute-start(bf16[2,256,1024]{2,1,0:T(8,128)(2,1)} %get-tuple-element.94), channel_id=1, source_target_pairs={{0,2},{1,3},{2,0},{3,1},{4,6},{5,7},{6,4},{7,5}} | collective-permute-start | bytes 3145736 | tf_op jit(solution)/shard_map/ppermute | solution.py:833
  406.5 46.2 %collective-permute-start.19 = (bf16[2,256,1024]{2,1,0:T(8,128)(2,1)}, bf16[2,256,1024]{2,1,0:T(8,128)(2,1)}, u32[]{:S(2)}, u32[]{:S(2)}) collective-permute-start(bf16[2,256,1024]{2,1,0:T(8,128)(2,1)} %get-tuple-element.95), channel_id=1, source_target_pairs={{0,3},{1,2},{2,1},{3,0},{4,7},{5,6},{6,5},{7,4}} | collective-permute-start | bytes 3145736 | tf_op jit(solution)/shard_map/ppermute | solution.py:833
  406.7 48.8 %collective-permute-start.23 = (bf16[256,4096]{1,0:T(8,128)(2,1)}, bf16[256,4096]{1,0:T(8,128)(2,1)}, u32[]{:S(2)}, u32[]{:S(2)}) collective-permute-start(bf16[256,4096]{1,0:T(8,128)(2,1)} %collective-permute-done.21.refs_6_), channel_id=1, source_target_pairs={{0,4},{4,0},{1,5},{5,1},{2,6},{6,2},{3,7},{7,3}} | collective-permute-start | bytes 6291464 | tf_op jit(solution)/shard_map/ppermute | solution.py:833
  407.8 92.0 %collective-permute-start.24 = (bf16[256,4096]{1,0:T(8,128)(2,1)}, bf16[256,4096]{1,0:T(8,128)(2,1)}, u32[]{:S(2)}, u32[]{:S(2)}) collective-permute-start(bf16[256,4096]{1,0:T(8,128)(2,1)} %collective-permute-done.22.refs_7_), channel_id=1, source_target_pairs={{0,4},{4,0},{1,5},{5,1},{2,6},{6,2},{3,7},{7,3}} | collective-permute-start | bytes 6291464 | tf_op jit(solution)/shard_map/ppermute | solution.py:833
  526.8 47.7 %collective-permute-start.25 = (bf16[256,4096]{1,0:T(8,128)(2,1)}, bf16[256,4096]{1,0:T(8,128)(2,1)}, u32[]{:S(2)}, u32[]{:S(2)}) collective-permute-start(bf16[256,4096]{1,0:T(8,128)(2,1)} %get-tuple-element.104.refs_0_), channel_id=1, source_target_pairs={{0,2},{1,3},{2,0},{3,1},{4,6},{5,7},{6,4},{7,5}} | collective-permute-start | bytes 6291464 | tf_op jit(solution)/shard_map/ppermute | solution.py:833
  572.3 92.6 %collective-permute-start.28 = (bf16[2,256,1024]{2,1,0:T(8,128)(2,1)}, bf16[2,256,1024]{2,1,0:T(8,128)(2,1)}, u32[]{:S(2)}, u32[]{:S(2)}) collective-permute-start(bf16[2,256,1024]{2,1,0:T(8,128)(2,1)} %get-tuple-element.115), channel_id=1, source_target_pairs={{0,1},{1,0},{2,3},{3,2},{4,5},{5,4},{6,7},{7,6}} | collective-permute-start | bytes 3145736 | tf_op jit(solution)/shard_map/ppermute | solution.py:833
  572.4 92.6 %collective-permute-start.29 = (bf16[2,256,1024]{2,1,0:T(8,128)(2,1)}, bf16[2,256,1024]{2,1,0:T(8,128)(2,1)}, u32[]{:S(2)}, u32[]{:S(2)}) collective-permute-start(bf16[2,256,1024]{2,1,0:T(8,128)(2,1)} %get-tuple-element.116), channel_id=1, source_target_pairs={{0,2},{1,3},{2,0},{3,1},{4,6},{5,7},{6,4},{7,5}} | collective-permute-start | bytes 3145736 | tf_op jit(solution)/shard_map/ppermute | solution.py:833
  572.4 92.6 %collective-permute-start.30 = (bf16[2,256,1024]{2,1,0:T(8,128)(2,1)}, bf16[2,256,1024]{2,1,0:T(8,128)(2,1)}, u32[]{:S(2)}, u32[]{:S(2)}) collective-permute-start(bf16[2,256,1024]{2,1,0:T(8,128)(2,1)} %get-tuple-element.117), channel_id=1, source_target_pairs={{0,3},{1,2},{2,1},{3,0},{4,7},{5,6},{6,5},{7,4}} | collective-permute-start | bytes 3145736 | tf_op jit(solution)/shard_map/ppermute | solution.py:833
  574.2 121.5 %collective-permute-start.27 = (bf16[256,4096]{1,0:T(8,128)(2,1)}, bf16[256,4096]{1,0:T(8,128)(2,1)}, u32[]{:S(2)}, u32[]{:S(2)}) collective-permute-start(bf16[256,4096]{1,0:T(8,128)(2,1)} %get-tuple-element.113.refs_0_), channel_id=1, source_target_pairs={{0,2},{1,3},{2,0},{3,1},{4,6},{5,7},{6,4},{7,5}} | collective-permute-start | bytes 6291464 | tf_op jit(solution)/shard_map/ppermute | solution.py:833
  691.9 143.7 %collective-permute-start.32 = (bf16[256,4096]{1,0:T(8,128)(2,1)}, bf16[256,4096]{1,0:T(8,128)(2,1)}, u32[]{:S(2)}, u32[]{:S(2)}) collective-permute-start(bf16[256,4096]{1,0:T(8,128)(2,1)} %get-tuple-element.122.refs_0_), channel_id=1, source_target_pairs={{0,2},{1,3},{2,0},{3,1},{4,6},{5,7},{6,4},{7,5}} | collective-permute-start | bytes 6291464 | tf_op jit(solution)/shard_map/ppermute | solution.py:833
  693.7 239.0 %collective-permute-start.34 = (bf16[256,4096]{1,0:T(8,128)(2,1)}, bf16[256,4096]{1,0:T(8,128)(2,1)}, u32[]{:S(2)}, u32[]{:S(2)}) collective-permute-start(bf16[256,4096]{1,0:T(8,128)(2,1)} %get-tuple-element.125.refs_0_), channel_id=1, source_target_pairs={{0,2},{1,3},{2,0},{3,1},{4,6},{5,7},{6,4},{7,5}} | collective-permute-start | bytes 6291464 | tf_op jit(solution)/shard_map/ppermute | solution.py:833
  694.0 136.7 %collective-permute-start.26 = (bf16[256,4096]{1,0:T(8,128)(2,1)}, bf16[256,4096]{1,0:T(8,128)(2,1)}, u32[]{:S(2)}, u32[]{:S(2)}) collective-permute-start(bf16[256,4096]{1,0:T(8,128)(2,1)} %get-tuple-element.112), channel_id=1, source_target_pairs={{0,2},{1,3},{2,0},{3,1},{4,6},{5,7},{6,4},{7,5}} | collective-permute-start | bytes 6291464 | tf_op jit(solution)/shard_map/ppermute | solution.py:833
  786.3 141.5 %collective-permute-start.31 = (bf16[256,4096]{1,0:T(8,128)(2,1)}, bf16[256,4096]{1,0:T(8,128)(2,1)}, u32[]{:S(2)}, u32[]{:S(2)}) collective-permute-start(bf16[256,4096]{1,0:T(8,128)(2,1)} %get-tuple-element.120), channel_id=1, source_target_pairs={{0,2},{1,3},{2,0},{3,1},{4,6},{5,7},{6,4},{7,5}} | collective-permute-start | bytes 6291464 | tf_op jit(solution)/shard_map/ppermute | solution.py:833
  926.0 56.7 %collective-permute-start.33 = (bf16[256,4096]{1,0:T(8,128)(2,1)}, bf16[256,4096]{1,0:T(8,128)(2,1)}, u32[]{:S(2)}, u32[]{:S(2)}) collective-permute-start(bf16[256,4096]{1,0:T(8,128)(2,1)} %get-tuple-element.124), channel_id=1, source_target_pairs={{0,2},{1,3},{2,0},{3,1},{4,6},{5,7},{6,4},{7,5}} | collective-permute-start | bytes 6291464 | tf_op jit(solution)/shard_map/ppermute | solution.py:833
  982.4 67.1 %collective-permute-start.35 = (bf16[128,4096]{1,0:T(8,128)(2,1)}, bf16[128,4096]{1,0:T(8,128)(2,1)}, u32[]{:S(2)}, u32[]{:S(2)}) collective-permute-start(bf16[128,4096]{1,0:T(8,128)(2,1)} %get-tuple-element.127), channel_id=1, source_target_pairs={{0,2},{1,3},{2,0},{3,1},{4,6},{5,7},{6,4},{7,5}} | collective-permute-start | bytes 3145736 | tf_op jit(solution)/shard_map/ppermute | solution.py:833
